TPU v7x, 32 devices: a whole 2x2x4 slice. The times are simulated.
32 devices in a mesh: tok: 8 (over z, core), mdl: 4 (over y, x).
Axes of the slice: x: 2, y: 2, z: 4, core: 2. Of those that a mesh axis runs over, the one named last changes fastest.
Arguments:
- inputs: bfloat16 [8192, 2560], P('tok', 'mdl'), may hold values from -6 to 6
- positions: int32 [8192], P(('tok', 'mdl')), may hold values from 0 to 1023, as said below
- norm1_gain: bfloat16 [2560], P('tok'), may hold values from 0.099609375 to 1.8984375
- qkv_weight: bfloat16 [2560, 3072], P('tok', 'mdl'), as said below
- out_weight: bfloat16 [2560, 2560], P('mdl', 'tok'), may hold values from -0.5 to 0.5
- norm2_gain: bfloat16 [2560], P('tok'), may hold values from 0.099609375 to 1.8984375
- gate_weight: bfloat16 [2560, 7680], P('tok', 'mdl'), may hold values from -0.125 to 0.125
- up_weight: bfloat16 [2560, 7680], P('tok', 'mdl'), may hold values from -0.125 to 0.125
- down_weight: bfloat16 [7680, 2560], P('mdl', 'tok'), may hold values from -0.0625 to 0.0625
- cotangent: bfloat16 [8192, 2560], P('tok'), may hold values from -6 to 6
Outputs:
- block_out: bfloat16 [8192, 2560], P('tok', 'mdl')
- input_grad: float32 [8192, 2560], P('tok', 'mdl')
- norm1_gain_grad: float32 [2560], P('tok')
- qkv_grad: float32 [2560, 3072], P('tok', 'mdl')
- out_grad: float32 [2560, 2560], P('mdl', 'tok')
- norm2_gain_grad: float32 [2560], P('tok')
- gate_grad: float32 [2560, 7680], P('tok', 'mdl')
- up_grad: float32 [2560, 7680], P('tok', 'mdl')
- down_grad: float32 [7680, 2560], P('mdl', 'tok')
Inputs may be any that keep to these rules, and one draw needn't show every extreme that they name: positions[t] is 0 where a packed sequence begins and positions[t-1] + 1 otherwise; every sequence lies inside one aligned block of 1024 tokens. `qkv_weight`: projection weights, columns in the order of the query heads, the key head and the value head.
All inputs are finite; a program needn't handle non-finite values.
Results may differ from a plain program's by a relative error of at most 0.023.
Values may be sent and summed in bfloat16 or wider, within the bound.
A program may use at most 320 MiB of HBM per device.

v0:
```python
import math

import jax
import jax.numpy as jnp
from jax import lax
from jax.sharding import PartitionSpec as P

HEADS = 10
HEAD = 256
SEG_MAX = 1024


norm_eps = 1e-06


def from_behind(block, axis, distance):
    devices = range(lax.axis_size(axis))
    route = [(i - distance, i) for i in devices if i - distance in devices]
    return lax.ppermute(block, axis, route)


def normalize(vector_rows, gain_row):
    return (
        vector_rows
        * lax.rsqrt(jnp.mean(vector_rows * vector_rows, axis=-1, keepdims=True) + norm_eps)
        * gain_row
    )


def gated_gelu(gate_in, up_in):
    return jax.nn.gelu(gate_in, approximate=True) * up_in


def rotary_tables(position_ids, head_width):
    half_width = head_width // 2
    frequency = jnp.exp(
        jnp.arange(half_width, dtype=jnp.float32) * (-2.0 * math.log(10000.0) / head_width)
    )
    angles = position_ids.astype(jnp.float32)[:, None] * frequency[None, :]
    return (jnp.cos(angles), jnp.sin(angles))


def rotate(vector, cos_table, sin_table):
    half_width = vector.shape[-1] // 2
    lower_half = vector[..., :half_width]
    upper_half = vector[..., half_width:]
    return jnp.concatenate(
        [
            lower_half * cos_table - upper_half * sin_table,
            upper_half * cos_table + lower_half * sin_table,
        ],
        axis=-1,
    )


def unrotate(vector, cos_table, sin_table):
    half_width = vector.shape[-1] // 2
    lower_half = vector[..., :half_width]
    upper_half = vector[..., half_width:]
    return jnp.concatenate(
        [
            lower_half * cos_table + upper_half * sin_table,
            upper_half * cos_table - lower_half * sin_table,
        ],
        axis=-1,
    )


def contract_last(left_op, right_op):
    return lax.dot_general(
        left_op, right_op, (((1,), (1,)), ((), ())), preferred_element_type=jnp.float32
    )


def contract_first(left_op, right_op):
    return lax.dot_general(
        left_op, right_op, (((0,), (0,)), ((), ())), preferred_element_type=jnp.float32
    )


def on_device(
    inputs,
    positions,
    norm1_gain,
    qkv_weight,
    out_weight,
    norm2_gain,
    gate_weight,
    up_weight,
    down_weight,
    cotangent,
):
    groups = lax.axis_size("mdl")
    col_index = lax.axis_index("mdl")
    full_rows = lax.all_gather(inputs, "mdl", axis=1, tiled=True)
    gain_one, w_qkv, w_out, gain_two, w_gate, w_up, w_down = (
        lax.all_gather(norm1_gain, "tok", axis=0, tiled=True),
        lax.all_gather(qkv_weight, "tok", axis=0, tiled=True),
        lax.all_gather(out_weight, "tok", axis=1, tiled=True),
        lax.all_gather(norm2_gain, "tok", axis=0, tiled=True),
        lax.all_gather(gate_weight, "tok", axis=0, tiled=True),
        lax.all_gather(up_weight, "tok", axis=0, tiled=True),
        lax.all_gather(down_weight, "tok", axis=1, tiled=True),
    )
    gain_one = gain_one.astype(jnp.float32)
    gain_two = gain_two.astype(jnp.float32)
    head_cols = HEADS * HEAD
    score_scale = HEAD ** (-0.5)
    residual = full_rows.astype(jnp.float32)
    normed_one = normalize(residual, gain_one).astype(jnp.bfloat16)
    qkv_part = jnp.dot(normed_one, w_qkv, preferred_element_type=jnp.float32).astype(jnp.bfloat16)
    qkv_rows = lax.all_to_all(qkv_part, "mdl", split_axis=0, concat_axis=1, tiled=True)
    query_count = qkv_rows.shape[0]
    reach = SEG_MAX // query_count - 1
    cos_table, sin_table = rotary_tables(positions, HEAD)
    query_rows = rotate(
        qkv_rows[:, :head_cols].astype(jnp.float32).reshape(query_count, HEADS, HEAD),
        cos_table[:, None, :],
        sin_table[:, None, :],
    )
    query_rows = (query_rows * score_scale).astype(jnp.bfloat16).reshape(query_count * HEADS, HEAD)
    key_rows = rotate(
        qkv_rows[:, head_cols : head_cols + HEAD].astype(jnp.float32), cos_table, sin_table
    ).astype(jnp.bfloat16)
    value_rows = qkv_rows[:, head_cols + HEAD :]
    key_parts = [key_rows]
    value_parts = [value_rows]
    for steps_back in range(1, reach + 1):
        moved_keys, moved_values = from_behind((key_rows, value_rows), "mdl", steps_back)
        key_parts.append(moved_keys)
        value_parts.append(moved_values)
    all_keys = jnp.concatenate(key_parts[::-1], axis=0)
    all_values = jnp.concatenate(value_parts[::-1], axis=0)
    first_key = (col_index - reach) * query_count
    key_count = all_keys.shape[0]
    query_index = col_index * query_count + jnp.arange(query_count, dtype=jnp.int32)
    key_index = first_key + jnp.arange(key_count, dtype=jnp.int32)
    distance = query_index[:, None] - key_index[None, :]
    visible = ((distance >= 0) & (distance <= positions[:, None]))[:, None, :]
    scores = contract_last(query_rows, all_keys).reshape(query_count, HEADS, key_count)
    masked = jnp.where(visible, scores, -jnp.inf)
    row_max = jnp.max(masked, axis=-1, keepdims=True)
    weights_exp = jnp.exp(masked - row_max)
    row_sum = jnp.sum(weights_exp, axis=-1, keepdims=True)
    log_norm = row_max + jnp.log(row_sum)
    attn_probs = (
        (weights_exp / row_sum).astype(jnp.bfloat16).reshape(query_count * HEADS, key_count)
    )
    attended = (
        jnp.dot(attn_probs, all_values, preferred_element_type=jnp.float32)
        .astype(jnp.bfloat16)
        .reshape(query_count, head_cols)
    )
    head_block = lax.all_to_all(attended, "mdl", split_axis=1, concat_axis=0, tiled=True)
    attn_part = jnp.dot(head_block, w_out, preferred_element_type=jnp.float32)
    mixed = residual + lax.psum(attn_part.astype(jnp.bfloat16), "mdl").astype(jnp.float32)
    normed_two = normalize(mixed, gain_two).astype(jnp.bfloat16)
    gate_in = jnp.dot(normed_two, w_gate, preferred_element_type=jnp.float32)
    up_in = jnp.dot(normed_two, w_up, preferred_element_type=jnp.float32)
    hidden = gated_gelu(gate_in, up_in).astype(jnp.bfloat16)
    ffn_part = jnp.dot(hidden, w_down, preferred_element_type=jnp.float32)
    ffn_share = lax.psum_scatter(
        ffn_part.astype(jnp.bfloat16), "mdl", scatter_dimension=1, tiled=True
    ).astype(jnp.float32)
    col_width = full_rows.shape[1] // groups
    mixed_share = lax.dynamic_slice_in_dim(mixed, col_index * col_width, col_width, 1)
    block_out = (mixed_share + ffn_share).astype(jnp.bfloat16)
    d_hidden = contract_last(cotangent, w_down)
    unused, gelu_back = jax.vjp(gated_gelu, gate_in, up_in)
    d_gate, d_up = gelu_back(d_hidden)
    d_gate = d_gate.astype(jnp.bfloat16)
    d_up = d_up.astype(jnp.bfloat16)
    grad_down = contract_first(hidden, cotangent)
    grad_gate = contract_first(normed_two, d_gate)
    grad_up = contract_first(normed_two, d_up)
    d_norm_two_part = contract_last(d_gate, w_gate) + contract_last(d_up, w_up)
    d_normed_two = lax.psum(d_norm_two_part.astype(jnp.bfloat16), "mdl").astype(jnp.float32)
    unused, norm_back = jax.vjp(normalize, mixed, gain_two)
    d_mixed, grad_gain_two = norm_back(d_normed_two)
    d_mixed = d_mixed + cotangent.astype(jnp.float32)
    d_mixed_b = d_mixed.astype(jnp.bfloat16)
    grad_out = contract_first(head_block, d_mixed_b)
    d_head_part = contract_last(d_mixed_b, w_out).astype(jnp.bfloat16)
    d_attended = lax.all_to_all(d_head_part, "mdl", split_axis=0, concat_axis=1, tiled=True)
    d_rows = d_attended.reshape(query_count * HEADS, HEAD)
    again_scores = contract_last(query_rows, all_keys).reshape(query_count, HEADS, key_count)
    again = jnp.exp(jnp.where(visible, again_scores, -jnp.inf) - log_norm)
    again_b = again.astype(jnp.bfloat16).reshape(query_count * HEADS, key_count)
    d_values_all = contract_first(again_b, d_rows)
    d_probs = contract_last(d_rows, all_values).reshape(query_count, HEADS, key_count)
    delta = jnp.sum(
        d_attended.astype(jnp.float32).reshape(query_count, HEADS, HEAD)
        * attended.astype(jnp.float32).reshape(query_count, HEADS, HEAD),
        axis=-1,
        keepdims=True,
    )
    d_scores = (
        (again * (d_probs - delta)).astype(jnp.bfloat16).reshape(query_count * HEADS, key_count)
    )
    d_queries = (
        jnp.dot(d_scores, all_keys, preferred_element_type=jnp.float32).reshape(
            query_count, HEADS, HEAD
        )
        * score_scale
    )
    d_keys_all = contract_first(d_scores, query_rows)
    own_start = reach * query_count
    key_grad = d_keys_all[own_start:]
    value_grad = d_values_all[own_start:]
    for steps_back in range(1, reach + 1):
        row_start = (reach - steps_back) * query_count
        got_keys, got_values = (
            from_behind(
                d_keys_all[row_start : row_start + query_count].astype(jnp.bfloat16),
                "mdl",
                -steps_back,
            ).astype(jnp.float32),
            from_behind(
                d_values_all[row_start : row_start + query_count].astype(jnp.bfloat16),
                "mdl",
                -steps_back,
            ).astype(jnp.float32),
        )
        key_grad = key_grad + got_keys
        value_grad = value_grad + got_values
    d_queries = unrotate(d_queries, cos_table[:, None, :], sin_table[:, None, :]).reshape(
        query_count, head_cols
    )
    key_grad = unrotate(key_grad, cos_table, sin_table)
    d_qkv = jnp.concatenate([d_queries, key_grad, value_grad], axis=1).astype(jnp.bfloat16)
    d_qkv_part = lax.all_to_all(d_qkv, "mdl", split_axis=1, concat_axis=0, tiled=True)
    grad_qkv = contract_first(normed_one, d_qkv_part)
    d_norm_one_part = contract_last(d_qkv_part, w_qkv)
    d_normed_one = lax.psum(d_norm_one_part.astype(jnp.bfloat16), "mdl").astype(jnp.float32)
    unused, norm_one_back = jax.vjp(normalize, residual, gain_one)
    d_residual, grad_gain_one = norm_one_back(d_normed_one)
    input_full = d_mixed + d_residual
    input_grad = lax.dynamic_slice_in_dim(input_full, col_index * col_width, col_width, 1)
    gain_one_sum, qkv_sum, out_sum, gain_two_sum, gate_sum, up_sum, down_sum = (
        lax.psum_scatter(
            grad_gain_one.astype(jnp.bfloat16), "tok", scatter_dimension=0, tiled=True
        ).astype(jnp.float32),
        lax.psum_scatter(
            grad_qkv.astype(jnp.bfloat16), "tok", scatter_dimension=0, tiled=True
        ).astype(jnp.float32),
        lax.psum_scatter(
            grad_out.astype(jnp.bfloat16), "tok", scatter_dimension=1, tiled=True
        ).astype(jnp.float32),
        lax.psum_scatter(
            grad_gain_two.astype(jnp.bfloat16), "tok", scatter_dimension=0, tiled=True
        ).astype(jnp.float32),
        lax.psum_scatter(
            grad_gate.astype(jnp.bfloat16), "tok", scatter_dimension=0, tiled=True
        ).astype(jnp.float32),
        lax.psum_scatter(
            grad_up.astype(jnp.bfloat16), "tok", scatter_dimension=0, tiled=True
        ).astype(jnp.float32),
        lax.psum_scatter(
            grad_down.astype(jnp.bfloat16), "tok", scatter_dimension=1, tiled=True
        ).astype(jnp.float32),
    )
    return (
        block_out,
        input_grad,
        gain_one_sum,
        qkv_sum,
        out_sum,
        gain_two_sum,
        gate_sum,
        up_sum,
        down_sum,
    )


def solution(mesh):
    placed = (
        P("tok", "mdl"),
        P(("tok", "mdl")),
        P("tok"),
        P("tok", "mdl"),
        P("mdl", "tok"),
        P("tok"),
        P("tok", "mdl"),
        P("tok", "mdl"),
        P("mdl", "tok"),
        P("tok", None),
    )
    return jax.shard_map(
        on_device,
        mesh=mesh,
        in_specs=placed,
        out_specs=(
            P("tok", "mdl"),
            P("tok", "mdl"),
            P("tok"),
            P("tok", "mdl"),
            P("mdl", "tok"),
            P("tok"),
            P("tok", "mdl"),
            P("tok", "mdl"),
            P("mdl", "tok"),
        ),
        check_vma=False,
    )
```

profile of v0, /device:TPU:0, one launch (start us, length us, event | category | flops | bytes accessed | tf_op | source)
XLA Modules:
  0.0 1463.7 jit_solution(4928322728736944927)
XLA Ops:
  12.4 30.3 %all-reduce.5 = (bf16[2560]{0:T(1024)(128)(2,1)S(1)}, bf16[2560]{0:T(1024)(128)(2,1)S(1)}) all-reduce(bf16[2560]{0:T(1024)(128)(2,1)S(1)} %dynamic-update-slice.1, bf16[2560]{0:T(1024)(128)(2,1)S(1)} %dynamic-update-slice), channel_id=1, replica_groups=mesh['tok'=8,'mdl'=4] {'tok'}, use_global_device_ids=true, to_apply=%add.1 | all-reduce | flops 5120 | bytes 20480
  42.7 31.2 %all-gather.7.cloned.1.call-done = bf16[1024,2560]{1,0:T(8,128)(2,1)} async-done(((bf16[1024,640]{1,0:T(8,128)(2,1)}), bf16[1024,2560]{1,0:T(8,128)(2,1)}) %all-gather.7.cloned.1.call-update) | async-done | bytes 5242896 | tf_op jit(solution)/shard_map/all_gather | solution.py:95
  73.9 3.6 multiply_reduce_fusion.2
  78.1 42.2 %all-gather.9.cloned.1.call-done = bf16[2560,768]{1,0:T(8,128)(2,1)} async-done(((bf16[320,768]{1,0:T(8,128)(2,1)}), bf16[2560,768]{1,0:T(8,128)(2,1)}) %all-gather.9.cloned.1.call-update) | async-done | bytes 3932176 | tf_op jit(solution)/shard_map/all_gather | solution.py:98
  120.3 9.1 convolution_convert_fusion.9
  129.4 3.7 all-to-all-start
  134.2 18.6 %all-to-all-done = bf16[4,256,768]{2,1,0:T(8,128)(2,1)S(1)} async-done(((bf16[4,256,768]{2,1,0:T(8,128)(2,1)}), bf16[4,256,768]{2,1,0:T(8,128)(2,1)S(1)}, u32[]{:S(2)}, u32[]{:S(2)}) %all-to-all-start) | async-done | bytes 1572896 | tf_op jit(solution)/shard_map/all_to_all | solution.py:112
  154.0 4.0 collective-permute-start
  160.0 2.5 collective-permute-start.2
  175.5 2.8 select_reduce_fusion
  178.3 2.6 fusion.6
  182.2 4.8 fusion.7
  187.0 6.7 copy.53
  193.7 10.7 reshape.225
  204.4 4.1 convolution_convert_fusion.8
  210.6 3.5 all-to-all-start.1
  214.4 15.4 %all-to-all-done.1 = bf16[256,4,640]{2,0,1:T(8,128)(2,1)S(1)} async-done(((bf16[256,4,640]{2,0,1:T(8,128)(2,1)}), bf16[256,4,640]{2,0,1:T(8,128)(2,1)S(1)}, u32[]{:S(2)}, u32[]{:S(2)}) %all-to-all-start.1) | async-done | bytes 1310752 | tf_op jit(solution)/shard_map/all_to_all | solution.py:154
  229.8 8.4 convolution_convert_fusion.4
  240.2 117.2 %all-reduce.10.cloned.1.call-done = bf16[1024,2560]{1,0:T(8,128)(2,1)} async-done(((bf16[1024,2560]{1,0:T(8,128)(2,1)}), bf16[1024,2560]{1,0:T(8,128)(2,1)}) %all-reduce.10.cloned.1.call-update) | async-done | bytes 5242896 | tf_op jit(solution)/shard_map/psum | solution.py:156
  357.4 5.9 multiply_reduce_fusion.1
  363.3 7.5 multiply_convert_fusion.1
  370.9 82.0 %all-gather.13.cloned.1.call-done = bf16[2560,1920]{1,0:T(8,128)(2,1)} async-done(((bf16[320,1920]{1,0:T(8,128)(2,1)}), bf16[2560,1920]{1,0:T(8,128)(2,1)}) %all-gather.13.cloned.1.call-update) | async-done | bytes 9830416 | tf_op jit(solution)/shard_map/all_gather | solution.py:101
  452.8 17.1 %fusion.66 = f32[1024,1920]{1,0:T(8,128)} fusion(bf16[1024,2560]{1,0:T(8,128)(2,1)} %multiply_convert_fusion.1, bf16[2560,1920]{1,0:T(8,128)(2,1)} %all-gather.13.cloned.1.call-done), kind=kOutput, calls=%fused_computation.130 | convolution fusion | flops 10066329600 | bytes 22937600 | tf_op jit(solution)/shard_map/dot_general | solution.py:158
  469.9 76.8 %all-gather.15.cloned.1.call-done = bf16[2560,1920]{1,0:T(8,128)(2,1)} async-done(((bf16[320,1920]{1,0:T(8,128)(2,1)}), bf16[2560,1920]{1,0:T(8,128)(2,1)}) %all-gather.15.cloned.1.call-update) | async-done | bytes 9830416 | tf_op jit(solution)/shard_map/all_gather | solution.py:102
  546.7 17.1 %fusion.67 = f32[1024,1920]{1,0:T(8,128)} fusion(bf16[1024,2560]{1,0:T(8,128)(2,1)} %multiply_convert_fusion.1, bf16[2560,1920]{1,0:T(8,128)(2,1)} %all-gather.15.cloned.1.call-done), kind=kOutput, calls=%fused_computation.131 | convolution fusion | flops 10066329600 | bytes 22937600 | tf_op jit(solution)/shard_map/dot_general | solution.py:159
  563.8 76.9 %all-gather.17.cloned.1.call-done = bf16[1920,2560]{0,1:T(8,128)(2,1)} async-done(((bf16[1920,320]{0,1:T(8,128)(2,1)}), bf16[1920,2560]{0,1:T(8,128)(2,1)}) %all-gather.17.cloned.1.call-update) | async-done | bytes 9830416 | tf_op jit(solution)/shard_map/all_gather | solution.py:103
  640.7 26.9 %multiply_convert_fusion.3 = (bf16[1024,1920]{1,0:T(8,128)(2,1)}, bf16[1024,1920]{1,0:T(8,128)(2,1)}, bf16[1024,1920]{1,0:T(8,128)(2,1)}) fusion(f32[1024,1920]{1,0:T(8,128)} %fusion.66, f32[1024,1920]{1,0:T(8,128)} %fusion.67, bf16[1024,2560]{1,0:T(8,128)(2,1)} %param.19, bf16[1920,2560]{0,1:T(8,128)(2,1)} %all-gather.17.cloned.1.call-done), kind=kOutput, calls=%fused_computation.38 | convolution fusion | flops 10117447680 | bytes 42598400 | tf_op jit(solution)/shard_map/dot_general | solution.py:70
  667.6 17.4 %fusion.68 = f32[1024,2560]{1,0:T(8,128)} fusion(bf16[1024,1920]{1,0:T(8,128)(2,1)} %get-tuple-element.18, bf16[2560,1920]{1,0:T(8,128)(2,1)} %all-gather.13.cloned.1.call-done), kind=kOutput, calls=%fused_computation.132 | convolution fusion | flops 10066329600 | bytes 24248320 | tf_op jit(solution)/shard_map/dot_general | solution.py:70
  685.0 17.5 %add_convert_fusion = bf16[1024,2560]{1,0:T(8,128)(2,1)} fusion(f32[1024,2560]{1,0:T(8,128)} %fusion.68, bf16[1024,1920]{1,0:T(8,128)(2,1)S(1)} %copy-done.40, bf16[2560,1920]{1,0:T(8,128)(2,1)} %all-gather.15.cloned.1.call-done), kind=kOutput, calls=%fused_computation.19 | convolution fusion | flops 10071572480 | bytes 29491200 | tf_op jit(solution)/shard_map/dot_general | solution.py:70
  702.6 16.6 %convolution_convert_fusion.3 = bf16[1024,2560]{1,0:T(8,128)(2,1)} fusion(bf16[1024,1920]{1,0:T(8,128)(2,1)} %get-tuple-element.19, bf16[1920,2560]{0,1:T(8,128)(2,1)} %all-gather.17.cloned.1.call-done), kind=kOutput, calls=%fused_computation.41 | convolution fusion | flops 10068951040 | bytes 19005440 | tf_op jit(solution)/shard_map/dot_general | solution.py:161
  719.1 7.9 copy.77
  727.0 94.9 %all-reduce.12.cloned.1.call-done = bf16[1024,2560]{1,0:T(8,128)(2,1)} async-done(((bf16[1024,2560]{1,0:T(8,128)(2,1)}), bf16[1024,2560]{1,0:T(8,128)(2,1)}) %all-reduce.12.cloned.1.call-update) | async-done | bytes 5242896 | tf_op jit(solution)/shard_map/psum | solution.py:177
  822.0 12.0 fusion.3
  834.0 13.2 fusion.5
  847.2 4.3 fusion.20
  852.9 3.5 all-to-all-start.2
  858.7 4.7 copy.57
  863.4 9.1 copy.64
  872.5 11.0 reshape.227
  883.4 10.0 convolution_convert_fusion.7
  895.8 7.2 multiply_convert_fusion
  903.1 3.2 convolution_multiply_fusion
  909.5 5.8 fusion.65
  921.5 2.8 reshape.228
  924.3 5.1 fusion.64
  935.1 3.7 collective-permute-done.10
  942.7 21.2 %all_to_all.70 = bf16[256,4,768]{2,0,1:T(8,128)(2,1)S(1)} all-to-all(bf16[256,4,768]{2,0,1:T(8,128)(2,1)S(1)} %copy.68), channel_id=1, replica_groups=mesh['tok'=8,'mdl'=4] {'mdl'}, dimensions={1} | all-to-all | bytes 3145728 | tf_op jit(solution)/shard_map/all_to_all | solution.py:231
  963.9 8.1 convolution_convert_fusion.5
  972.8 9.4 convolution_convert_fusion.6
  982.3 16.8 %convolution_convert_fusion.2 = bf16[2560,1920]{1,0:T(8,128)(2,1)} fusion(bf16[1024,2560]{1,0:T(8,128)(2,1)} %multiply_convert_fusion.1, bf16[1024,1920]{1,0:T(8,128)(2,1)} %get-tuple-element.18), kind=kOutput, calls=%fused_computation.9 | convolution fusion | flops 10071244800 | bytes 19005440 | tf_op jit(solution)/shard_map/dot_general | solution.py:76
  999.1 16.6 %convolution_convert_fusion.1 = bf16[2560,1920]{1,0:T(8,128)(2,1)} fusion(bf16[1024,2560]{1,0:T(8,128)(2,1)} %multiply_convert_fusion.1, bf16[1024,1920]{1,0:T(8,128)(2,1)} %get-tuple-element.17), kind=kOutput, calls=%fused_computation.8 | convolution fusion | flops 10071244800 | bytes 19005440 | tf_op jit(solution)/shard_map/dot_general | solution.py:76
  1015.8 16.6 %convolution_convert_fusion = bf16[1920,2560]{0,1:T(8,128)(2,1)} fusion(bf16[1024,1920]{1,0:T(8,128)(2,1)} %get-tuple-element.19, bf16[1024,2560]{1,0:T(8,128)(2,1)} %param.19), kind=kOutput, calls=%fused_computation.7 | convolution fusion | flops 10071244800 | bytes 19005440 | tf_op jit(solution)/shard_map/dot_general | solution.py:76
  1033.1 8.6 convert_element_type.170
  1043.4 3.1 add_convert_fusion.1
  1048.4 44.2 %all-reduce.14.cloned.1.call-done = bf16[1024,2560]{1,0:T(8,128)(2,1)} async-done(((bf16[1024,2560]{1,0:T(8,128)(2,1)}), bf16[1024,2560]{1,0:T(8,128)(2,1)}) %all-reduce.14.cloned.1.call-update) | async-done | bytes 5242896 | tf_op jit(solution)/shard_map/psum | solution.py:234
  1092.5 12.3 fusion.4
  1104.8 30.1 %all-reduce.4 = (bf16[2560]{0:T(1024)(128)(2,1)S(1)}, bf16[2560]{0:T(1024)(128)(2,1)S(1)}) all-reduce(bf16[2560]{0:T(1024)(128)(2,1)S(1)} %get-tuple-element.11, bf16[2560]{0:T(1024)(128)(2,1)S(1)} %copy-done.30), channel_id=3, replica_groups=mesh['tok'=8,'mdl'=4] {'tok'}, use_global_device_ids=true, to_apply=%region_12.13.clone | all-reduce | flops 5120 | bytes 20480
  1135.7 5.4 fusion.15
  1144.8 101.6 %reduce-scatter.13.cloned.1.call-done = bf16[320,1920]{1,0:T(8,128)(2,1)} async-done(((bf16[2560,1920]{1,0:T(8,128)(2,1)}), bf16[320,1920]{1,0:T(8,128)(2,1)}) %reduce-scatter.13.cloned.1.call-update) | async-done | bytes 1228816 | tf_op jit(solution)/shard_map/reduce_scatter | solution.py:252
  1246.4 2.9 convert_element_type.217
  1249.3 100.9 %reduce-scatter.15.cloned.1.call-done = bf16[320,1920]{1,0:T(8,128)(2,1)} async-done(((bf16[2560,1920]{1,0:T(8,128)(2,1)}), bf16[320,1920]{1,0:T(8,128)(2,1)}) %reduce-scatter.15.cloned.1.call-update) | async-done | bytes 1228816 | tf_op jit(solution)/shard_map/reduce_scatter | solution.py:255
  1350.3 2.9 convert_element_type.219
  1353.1 100.9 %reduce-scatter.17.cloned.1.call-done = bf16[1920,320]{0,1:T(8,128)(2,1)} async-done(((bf16[1920,2560]{0,1:T(8,128)(2,1)}), bf16[1920,320]{0,1:T(8,128)(2,1)}) %reduce-scatter.17.cloned.1.call-update) | async-done | bytes 1228816 | tf_op jit(solution)/shard_map/reduce_scatter | solution.py:258
  1454.1 2.9 convert_element_type.221
  (187 shorter events, 61.6 us)
Async XLA Ops:
  7.2 66.7 %all-gather.7.cloned.1.call-start = ((), (), s32[]{:S(2)}) async-start(), calls=%async_computation.10 | async-start | bytes 6553600 | tf_op jit(solution)/shard_map/all_gather | solution.py:95
  7.9 112.4 %all-gather.9.cloned.1.call-start = ((), (), s32[]{:S(2)}) async-start(), calls=%async_computation.11 | async-start | bytes 4423680 | tf_op jit(solution)/shard_map/all_gather | solution.py:98
  42.7 86.7 %copy-start.24 = (f32[2560]{0:T(1024)}, f32[2560]{0:T(1024)S(1)}, u32[]{:S(2)}) copy-start(f32[2560]{0:T(1024)S(1)} %convert_element_type.171) | copy-start | bytes 30724
  78.1 51.3 %copy-start.26 = (f32[1024]{0:T(1024)}, f32[1024]{0:T(1024)S(1)}, u32[]{:S(2)}) copy-start(f32[1024]{0:T(1024)S(1)} %fusion.49) | copy-start | bytes 12292
  78.1 55.7 %copy-start.33 = (s32[256]{0:T(256)S(1)}, s32[256]{0:T(256)}, u32[]{:S(2)}) copy-start(s32[256]{0:T(256)} %param.11) | copy-start | bytes 3076
  129.4 23.5 %all-to-all-start = ((bf16[4,256,768]{2,1,0:T(8,128)(2,1)}), bf16[4,256,768]{2,1,0:T(8,128)(2,1)S(1)}, u32[]{:S(2)}, u32[]{:S(2)}) async-start(bf16[4,256,768]{2,1,0:T(8,128)(2,1)} %bitcast.1), calls=%async_computation | async-start | bytes 3145728 | tf_op jit(solution)/shard_map/all_to_all | solution.py:112
  133.0 81.4 %all-gather.11.cloned.1.call-start = ((), (), s32[]{:S(2)}) async-start(), calls=%async_computation.12 | async-start | bytes 3686400 | tf_op jit(solution)/shard_map/all_gather | solution.py:99
  133.8 20.2 %copy-start.31 = (f32[256]{0:T(256)}, f32[256]{0:T(256)S(1)}, u32[]{:S(2)}) copy-start(f32[256]{0:T(256)S(1)} %convert_element_type.174) | copy-start | bytes 3076
  133.8 20.2 %copy-start.34 = (f32[128]{0:T(128)}, f32[128]{0:T(128)S(1)}, u32[]{:S(2)}) copy-start(f32[128]{0:T(128)S(1)} %multiply_exponential_fusion) | copy-start | bytes 1540
  134.2 46.7 %copy-start.6 = (pred[256,1024]{1,0:T(8,128)(4,1)}, pred[256,1024]{1,0:T(8,128)(4,1)S(1)}, u32[]{:S(2)}) copy-start(pred[256,1024]{1,0:T(8,128)(4,1)S(1)} %fusion.23) | copy-start | bytes 786436
  153.4 51.0 %copy-start.20 = (bf16[256,256]{1,0:T(8,128)(2,1)}, bf16[256,256]{1,0:T(8,128)(2,1)S(1)}, u32[]{:S(2)}) copy-start(bf16[256,256]{1,0:T(8,128)(2,1)S(1)} %get-tuple-element.31) | copy-start | bytes 393220
  153.9 18.3 %copy-start.12 = (f32[256,128]{1,0:T(8,128)}, f32[256,128]{1,0:T(8,128)S(1)}, u32[]{:S(2)}) copy-start(f32[256,128]{1,0:T(8,128)S(1)} %get-tuple-element.43) | copy-start | bytes 393220
  154.0 18.3 %copy-start.14 = (f32[256,128]{1,0:T(8,128)}, f32[256,128]{1,0:T(8,128)S(1)}, u32[]{:S(2)}) copy-start(f32[256,128]{1,0:T(8,128)S(1)} %get-tuple-element.44) | copy-start | bytes 393220
  154.0 21.5 %copy-start.16 = (bf16[256,128]{1,0:T(8,128)(2,1)}, bf16[256,128]{1,0:T(8,128)(2,1)S(1)}, u32[]{:S(2)}) copy-start(bf16[256,128]{1,0:T(8,128)(2,1)S(1)} %get-tuple-element.45) | copy-start | bytes 196612
  154.0 21.5 %copy-start.18 = (bf16[256,128]{1,0:T(8,128)(2,1)}, bf16[256,128]{1,0:T(8,128)(2,1)S(1)}, u32[]{:S(2)}) copy-start(bf16[256,128]{1,0:T(8,128)(2,1)S(1)} %get-tuple-element.46) | copy-start | bytes 196612
  154.0 19.9 %collective-permute-start = (bf16[256,256]{1,0:T(8,128)(2,1)S(1)}, bf16[256,256]{1,0:T(8,128)(2,1)}, u32[]{:S(2)}, u32[]{:S(2)}) collective-permute-start(bf16[256,256]{1,0:T(8,128)(2,1)S(1)} %pad_maximum_fusion.3), channel_id=1, source_target_pairs={{0,3},{4,7},{8,11},{12,15},{16,19},{20,23},{24,27},{28,31}} | collective-permute-start | bytes 393224 | tf_op jit(solution)/shard_map/ppermute | solution.py:19
  158.0 17.4 %collective-permute-start.1 = (bf16[256,256]{1,0:T(8,128)(2,1)S(1)}, bf16[256,256]{1,0:T(8,128)(2,1)}, u32[]{:S(2)}, u32[]{:S(2)}) collective-permute-start(bf16[256,256]{1,0:T(8,128)(2,1)S(1)} %pad_maximum_fusion.3), channel_id=1, source_target_pairs={{0,2},{1,3},{4,6},{5,7},{8,10},{9,11},{12,14},{13,15},{16,18},{17,... | collective-permute-start | bytes 393224 | tf_op jit(solution)/shard_map/ppermute | solution.py:19
  160.0 15.5 %collective-permute-start.2 = (bf16[256,256]{1,0:T(8,128)(2,1)S(1)}, bf16[256,256]{1,0:T(8,128)(2,1)}, u32[]{:S(2)}, u32[]{:S(2)}) collective-permute-start(bf16[256,256]{1,0:T(8,128)(2,1)S(1)} %pad_maximum_fusion.3), channel_id=1, source_target_pairs={{0,1},{1,2},{2,3},{4,5},{5,6},{6,7},{8,9},{9,10},{10,11},{12,13},{... | collective-permute-start | bytes 393224 | tf_op jit(solution)/shard_map/ppermute | solution.py:19
  162.4 42.0 %collective-permute-start.3 = (bf16[256,256]{1,0:T(8,128)(2,1)S(1)}, bf16[256,256]{1,0:T(8,128)(2,1)}, u32[]{:S(2)}, u32[]{:S(2)}) collective-permute-start(bf16[256,256]{1,0:T(8,128)(2,1)S(1)} %get-tuple-element.31), channel_id=1, source_target_pairs={{0,3},{4,7},{8,11},{12,15},{16,19},{20,23},{24,27},{28,31}} | collective-permute-start | bytes 393224 | tf_op jit(solution)/shard_map/ppermute | solution.py:19
  164.4 40.0 %collective-permute-start.4 = (bf16[256,256]{1,0:T(8,128)(2,1)S(1)}, bf16[256,256]{1,0:T(8,128)(2,1)}, u32[]{:S(2)}, u32[]{:S(2)}) collective-permute-start(bf16[256,256]{1,0:T(8,128)(2,1)S(1)} %get-tuple-element.31), channel_id=1, source_target_pairs={{0,2},{1,3},{4,6},{5,7},{8,10},{9,11},{12,14},{13,15},{16,18},{17,... | collective-permute-start | bytes 393224 | tf_op jit(solution)/shard_map/ppermute | solution.py:19
  173.9 4.3 copy-start.10
  173.9 4.3 copy-start.11
  174.0 30.4 %collective-permute-start.5 = (bf16[256,256]{1,0:T(8,128)(2,1)S(1)}, bf16[256,256]{1,0:T(8,128)(2,1)S(1)}, u32[]{:S(2)}, u32[]{:S(2)}) collective-permute-start(bf16[256,256]{1,0:T(8,128)(2,1)S(1)} %get-tuple-element.31), channel_id=1, source_target_pairs={{0,1},{1,2},{2,3},{4,5},{5,6},{6,7},{8,9},{9,10},{10,11},{12,13},{... | collective-permute-start | bytes 393224 | tf_op jit(solution)/shard_map/ppermute | solution.py:19
  178.3 3.9 copy-start.1
  182.1 4.8 copy-start.22
  204.4 4.1 copy-start.37
  208.5 29.7 %copy-start.4 = (bf16[2560,256]{1,0:T(8,128)(2,1)}, bf16[2560,256]{1,0:T(8,128)(2,1)S(1)}, u32[]{:S(2)}) copy-start(bf16[2560,256]{1,0:T(8,128)(2,1)S(1)} %convolution_convert_fusion.8) | copy-start | bytes 3932164
  210.6 19.3 %all-to-all-start.1 = ((bf16[256,4,640]{2,0,1:T(8,128)(2,1)}), bf16[256,4,640]{2,0,1:T(8,128)(2,1)S(1)}, u32[]{:S(2)}, u32[]{:S(2)}) async-start(bf16[256,4,640]{2,0,1:T(8,128)(2,1)} %copy.54), calls=%async_computation.1 | async-start | bytes 2621440 | tf_op jit(solution)/shard_map/all_to_all | solution.py:154
  214.1 143.3 %all-reduce.10.cloned.1.call-start = ((), (), s32[]{:S(2)}) async-start(), calls=%async_computation.13 | async-start | bytes 10485760 | tf_op jit(solution)/shard_map/psum | solution.py:156
  229.8 8.4 copy-start.8
  238.2 214.6 %all-gather.13.cloned.1.call-start = ((), (), s32[]{:S(2)}) async-start(), calls=%async_computation.14 | async-start | bytes 11059200 | tf_op jit(solution)/shard_map/all_gather | solution.py:101
  238.8 307.9 %all-gather.15.cloned.1.call-start = ((), (), s32[]{:S(2)}) async-start(), calls=%async_computation.15 | async-start | bytes 11059200 | tf_op jit(solution)/shard_map/all_gather | solution.py:102
  239.4 401.3 %all-gather.17.cloned.1.call-start = ((), (), s32[]{:S(2)}) async-start(), calls=%async_computation.16 | async-start | bytes 11059200 | tf_op jit(solution)/shard_map/all_gather | solution.py:103
  240.1 581.8 %all-reduce.12.cloned.1.call-start = ((), (), s32[]{:S(2)}) async-start(), calls=%async_computation.17 | async-start | bytes 10485760 | tf_op jit(solution)/shard_map/psum | solution.py:177
  357.4 6.0 copy-start
  667.6 17.4 %copy-start.40 = (bf16[1024,1920]{1,0:T(8,128)(2,1)S(1)}, bf16[1024,1920]{1,0:T(8,128)(2,1)}, u32[]{:S(2)}) copy-start(bf16[1024,1920]{1,0:T(8,128)(2,1)} %get-tuple-element.17) | copy-start | bytes 11796484
  702.5 339.2 %reduce-scatter.19.cloned.1.call-start = ((), (), s32[]{:S(2)}) async-start(), calls=%async_computation.24 | async-start | bytes 6553600
  822.0 12.0 copy-start.2
  834.0 13.2 copy-start.36
  847.2 4.3 copy-start.3
  851.4 5.1 copy-start.5
  852.9 40.6 %all-to-all-start.2 = ((bf16[4,256,640]{1,2,0:T(8,128)(2,1)}), bf16[4,256,640]{1,2,0:T(8,128)(2,1)S(1)}, u32[]{:S(2)}, u32[]{:S(2)}) async-start(bf16[4,256,640]{1,2,0:T(8,128)(2,1)} %copy.55), calls=%async_computation.2 | async-start | bytes 2621440 | tf_op jit(solution)/shard_map/all_to_all | solution.py:184
  856.5 190.0 %reduce-scatter.11.cloned.1.call-start = ((), (), s32[]{:S(2)}) async-start(), calls=%async_computation.20 | async-start | bytes 3686400 | tf_op jit(solution)/shard_map/reduce_scatter | solution.py:246
  872.5 11.0 copy-start.9
  893.5 199.0 %all-reduce.14.cloned.1.call-start = ((), (), s32[]{:S(2)}) async-start(), calls=%async_computation.18 | async-start | bytes 10485760 | tf_op jit(solution)/shard_map/psum | solution.py:234
  895.8 7.3 copy-start.17
  895.8 7.3 copy-start.19
  903.0 3.3 copy-start.39
  903.1 3.3 copy-start.13
  903.1 3.3 copy-start.15
  915.4 16.6 %collective-permute-start.6 = (bf16[256,256]{1,0:T(8,128)(2,1)S(1)}, bf16[256,256]{1,0:T(8,128)(2,1)S(1)}, u32[]{:S(2)}, u32[]{:S(2)}) collective-permute-start(bf16[256,256]{1,0:T(8,128)(2,1)S(1)} %get-tuple-element.33), channel_id=1, source_target_pairs={{1,0},{2,1},{3,2},{5,4},{6,5},{7,6},{9,8},{10,9},{11,10},{13,12},{... | collective-permute-start | bytes 393224 | tf_op jit(solution)/shard_map/ppermute | solution.py:19
  916.7 16.6 %collective-permute-start.7 = (bf16[256,256]{1,0:T(8,128)(2,1)S(1)}, bf16[256,256]{1,0:T(8,128)(2,1)S(1)}, u32[]{:S(2)}, u32[]{:S(2)}) collective-permute-start(bf16[256,256]{1,0:T(8,128)(2,1)S(1)} %get-tuple-element.35), channel_id=1, source_target_pairs={{2,0},{3,1},{6,4},{7,5},{10,8},{11,9},{14,12},{15,13},{18,16},{19,... | collective-permute-start | bytes 393224 | tf_op jit(solution)/shard_map/ppermute | solution.py:19
  918.0 15.3 %collective-permute-start.8 = (bf16[256,256]{1,0:T(8,128)(2,1)S(1)}, bf16[256,256]{1,0:T(8,128)(2,1)S(1)}, u32[]{:S(2)}, u32[]{:S(2)}) collective-permute-start(bf16[256,256]{1,0:T(8,128)(2,1)S(1)} %get-tuple-element.34), channel_id=1, source_target_pairs={{3,0},{7,4},{11,8},{15,12},{19,16},{23,20},{27,24},{31,28}} | collective-permute-start | bytes 393224 | tf_op jit(solution)/shard_map/ppermute | solution.py:19
  924.2 10.1 copy-start.32
  924.2 10.1 copy-start.35
  929.4 9.5 collective-permute-start.10
  930.7 10.2 collective-permute-start.11
  932.0 8.9 collective-permute-start.9
  972.1 170.7 %reduce-scatter.9.cloned.1.call-start = ((), (), s32[]{:S(2)}) async-start(), calls=%async_computation.19 | async-start | bytes 4423680 | tf_op jit(solution)/shard_map/reduce_scatter | solution.py:243
  982.2 264.2 %reduce-scatter.13.cloned.1.call-start = ((), (), s32[]{:S(2)}) async-start(), calls=%async_computation.21 | async-start | bytes 11059200 | tf_op jit(solution)/shard_map/reduce_scatter | solution.py:252
  999.0 351.2 %reduce-scatter.15.cloned.1.call-start = ((), (), s32[]{:S(2)}) async-start(), calls=%async_computation.22 | async-start | bytes 11059200 | tf_op jit(solution)/shard_map/reduce_scatter | solution.py:255
  1015.7 438.4 %reduce-scatter.17.cloned.1.call-start = ((), (), s32[]{:S(2)}) async-start(), calls=%async_computation.23 | async-start | bytes 11059200 | tf_op jit(solution)/shard_map/reduce_scatter | solution.py:258
  1048.4 56.5 %copy-start.30 = (bf16[2560]{0:T(1024)(128)(2,1)S(1)}, bf16[2560]{0:T(1024)(128)(2,1)}, u32[]{:S(2)}) copy-start(bf16[2560]{0:T(1024)(128)(2,1)} %get-tuple-element.9) | copy-start | bytes 15364
  1048.4 87.3 %copy-start.29 = (f32[1024]{0:T(1024)S(1)}, f32[1024]{0:T(1024)}, u32[]{:S(2)}) copy-start(f32[1024]{0:T(1024)} %copy-done.28) | copy-start | bytes 12292
  (7 other events, 11.1 us)
Sparse Core Ops, SparseCore 0:
  9.8 64.0 all-gather.6
  75.5 44.6 all-gather.8
  135.5 38.7 all-gather.10
  238.3 118.9 all-reduce.9
  358.9 93.9 all-gather.12
  454.3 92.3 all-gather.14
  548.4 92.3 all-gather.16
  702.6 119.2 all-reduce.11
  825.0 70.3 reduce-scatter.18
  897.5 41.2 reduce-scatter.10
  972.2 120.3 all-reduce.13
  1094.7 48.0 reduce-scatter.8
  1145.1 101.2 reduce-scatter.12
  1248.6 101.5 reduce-scatter.14
  1352.4 101.5 reduce-scatter.16
where the time goes:
time: 1470 us; the launch traced here: 1460 us
  waiting for transfers between devices  914 us (62%)
  matrix products  240 us (16%)
  other arithmetic  102 us (7%)
  blocking collectives  81.6 us (6%)
  local copies, waits for them, and re-layouts  76.6 us (5%)
  starting transfers between devices  33 us (2%)
  between operations  16.3 us (1%)
    psum x1, waiting for transfers between devices, on_device(): lax.psum(attn_part.astype(jnp.bfloat16), 'mdl').astype(jnp.float32)  117 us
    reduce_scatter x1, waiting for transfers between devices, on_device(): lax.psum_scatter(grad_gate.astype(jnp.bfloat16), 'tok', scatter_dimension...  102 us
    reduce_scatter x1, waiting for transfers between devices, on_device(): lax.psum_scatter(grad_up.astype(jnp.bfloat16), 'tok', scatter_dimension=0...  101 us
    reduce_scatter x1, waiting for transfers between devices, on_device(): lax.psum_scatter(grad_down.astype(jnp.bfloat16), 'tok', scatter_dimension...  101 us
    psum x1, waiting for transfers between devices, on_device(): lax.psum(d_norm_two_part.astype(jnp.bfloat16), 'mdl').astype(jnp.float32)  94.9 us
    dot_general x7, matrix products, contract_last(): lax.dot_general(left_op, right_op, (((1,), (1,)), ((), ())), preferred_el...  84.1 us
    all_gather x1, waiting for transfers between devices, on_device(): lax.all_gather(gate_weight, 'tok', axis=0, tiled=True)  82 us
    dot_general x7, matrix products, contract_first(): lax.dot_general(left_op, right_op, (((0,), (0,)), ((), ())), preferred_el...  80.4 us
  transfers between devices with their start and end apart: 30, of which 16 were waited for; matrix products, arithmetic and copies ran while one was open for 23% of the time, Pallas kernels for 0%

commit v1 on v0

v1 whole, which is shorter than its diff:
```python
import math

import jax
import jax.numpy as jnp
from jax import lax
from jax.experimental import pallas as pl
from jax.experimental.pallas import tpu as pltpu
from jax.sharding import PartitionSpec as P


HEADS = 10
HEAD = 256
NORM_EPS = 1e-06
F32 = jnp.float32
BF16 = jnp.bfloat16
MASKED = -1e30


def nt(left_op, right_op):
    return lax.dot_general(
        left_op, right_op, (((1,), (1,)), ((), ())), preferred_element_type=F32
    )


def tn(left_op, right_op):
    return lax.dot_general(
        left_op, right_op, (((0,), (0,)), ((), ())), preferred_element_type=F32
    )


def nn(left_op, right_op):
    return jnp.dot(left_op, right_op, preferred_element_type=F32)


def swap(block, distance):
    size = lax.axis_size("mdl")
    return lax.ppermute(block, "mdl", [(i, i ^ distance) for i in range(size)])


def gather_mdl(block, dim):
    size = lax.axis_size("mdl")
    if size != 4:
        return lax.all_gather(block, "mdl", axis=dim, tiled=True)
    me = lax.axis_index("mdl")
    half = block.shape[0] // 2
    along_x = swap(block, 1)
    along_y = swap(block, 2)
    top = swap(along_x[:half], 2)
    bottom = swap(along_y[half:], 1)
    width = block.shape[dim]
    shape = list(block.shape)
    shape[dim] = width * size
    whole = jnp.zeros(shape, block.dtype)

    def put(whole, piece, source, row):
        start = [0, 0]
        start[dim] = source * width
        start[0] = start[0] + row
        return lax.dynamic_update_slice(whole, piece, tuple(start))

    whole = put(whole, block, me, 0)
    whole = put(whole, along_x, me ^ 1, 0)
    whole = put(whole, along_y, me ^ 2, 0)
    whole = put(whole, top, me ^ 3, 0)
    whole = put(whole, bottom, me ^ 3, half)
    return whole


def scatter_mdl(part, dim):
    size = lax.axis_size("mdl")
    if size != 4:
        return lax.psum_scatter(part, "mdl", scatter_dimension=dim, tiled=True).astype(F32)
    me = lax.axis_index("mdl")
    shape = list(part.shape)
    shape[dim] //= size
    half = shape[0] // 2

    def piece(block, row):
        start = [0, 0]
        start[dim] = block * shape[dim]
        start[0] = start[0] + row
        return lax.dynamic_slice(part, tuple(start), (half, shape[1]))

    sums = []
    for row, first, second in ((0, 1, 2), (half, 2, 1)):
        sent = jnp.stack([piece(me ^ first, row), piece(me ^ 3, row)])
        sums.append((row, second, swap(sent, first)))
    partial = []
    for row, second, got in sums:
        other = piece(me ^ second, row).astype(F32) + got[1].astype(F32)
        partial.append((row, got[0], swap(other.astype(BF16), second)))
    return jnp.concatenate(
        [
            piece(me, row).astype(F32) + first.astype(F32) + second.astype(F32)
            for row, first, second in partial
        ],
        axis=0,
    )


def sum_mdl(value):
    size = lax.axis_size("mdl")
    distance = 1
    while distance < size:
        value = value + swap(value, distance)
        distance *= 2
    return value


def rows_to_cols(block):
    return lax.all_to_all(block, "mdl", split_axis=0, concat_axis=1, tiled=True)


def cols_to_rows(block):
    return lax.all_to_all(block, "mdl", split_axis=1, concat_axis=0, tiled=True)


def turn(vector, cos, sin):
    half = HEAD // 2
    lower, upper = vector[:, :half], vector[:, half:]
    return jnp.concatenate([lower * cos - upper * sin, upper * cos + lower * sin], axis=1)


def unturn(vector, cos, sin):
    half = HEAD // 2
    lower, upper = vector[:, :half], vector[:, half:]
    return jnp.concatenate([lower * cos + upper * sin, upper * cos - lower * sin], axis=1)


def seen(first_ref, position_ref, queries, keys):
    row = lax.broadcasted_iota(jnp.int32, (queries, keys), 0) + first_ref[0]
    distance = row - lax.broadcasted_iota(jnp.int32, (queries, keys), 1)
    return (distance >= 0) & (distance <= position_ref[...])


def forward_kernel(first_ref, q_ref, kv_ref, cos_ref, sin_ref, pos_ref, out_ref, norm_ref):
    query = turn(q_ref[...].astype(F32), cos_ref[...], sin_ref[...])
    query = (query * HEAD ** (-0.5)).astype(BF16)
    keys, values = kv_ref[:, :HEAD], kv_ref[:, HEAD:]
    scores = nt(query, keys)
    scores = jnp.where(seen(first_ref, pos_ref, *scores.shape), scores, MASKED)
    top = jnp.max(scores, axis=1, keepdims=True)
    weights = jnp.exp(scores - top)
    total = jnp.sum(weights, axis=1, keepdims=True)
    out_ref[...] = (nn(weights.astype(BF16), values) / total).astype(BF16)
    norm_ref[0] = top + jnp.log(total)


def backward_kernel(
    first_ref, q_ref, kv_ref, cos_ref, sin_ref, pos_ref, att_ref, datt_ref, norm_ref,
    dq_ref, dkv_ref,
):
    head = pl.program_id(0)
    scale = HEAD ** (-0.5)
    cos, sin = cos_ref[...], sin_ref[...]
    query = (turn(q_ref[...].astype(F32), cos, sin) * scale).astype(BF16)
    keys, values = kv_ref[:, :HEAD], kv_ref[:, HEAD:]
    scores = nt(query, keys)
    visible = seen(first_ref, pos_ref, *scores.shape)
    again = jnp.where(visible, jnp.exp(scores - norm_ref[0]), 0.0)
    d_att = datt_ref[...]
    delta = jnp.sum(d_att.astype(F32) * att_ref[...].astype(F32), axis=1, keepdims=True)
    d_scores = (again * (nt(d_att, values) - delta)).astype(BF16)
    d_query = nn(d_scores, keys) * scale
    dq_ref[...] = unturn(d_query, cos, sin).astype(BF16)

    @pl.when(head == 0)
    def _():
        dkv_ref[...] = jnp.zeros_like(dkv_ref)

    dkv_ref[:, :HEAD] += tn(d_scores, query)
    dkv_ref[:, HEAD:] += tn(again.astype(BF16), d_att)


def whole_spec(shape):
    return pl.BlockSpec(shape, lambda head: (0,) * len(shape))


def attention_forward(first, qkv, kv, cos, sin, pos):
    rows, keys = qkv.shape[0], kv.shape[0]
    head_spec = pl.BlockSpec((rows, HEAD), lambda head: (0, head))
    return pl.pallas_call(
        forward_kernel,
        grid=(HEADS,),
        out_shape=(
            jax.ShapeDtypeStruct((rows, HEADS * HEAD), BF16),
            jax.ShapeDtypeStruct((HEADS, rows, 1), F32),
        ),
        in_specs=[
            pl.BlockSpec(memory_space=pltpu.SMEM),
            head_spec,
            whole_spec((keys, 2 * HEAD)),
            whole_spec((rows, HEAD // 2)),
            whole_spec((rows, HEAD // 2)),
            whole_spec((rows, 1)),
        ],
        out_specs=(head_spec, pl.BlockSpec((1, rows, 1), lambda head: (head, 0, 0))),
        compiler_params=pltpu.CompilerParams(
            dimension_semantics=("arbitrary",), vmem_limit_bytes=32 << 20
        ),
        cost_estimate=pl.CostEstimate(
            flops=4 * rows * keys * HEADS * HEAD,
            bytes_accessed=4 * rows * HEADS * HEAD + 4 * keys * HEAD,
            transcendentals=rows * keys * HEADS,
        ),
        name="attention_forward",
    )(first, qkv, kv, cos, sin, pos)


def attention_backward(first, qkv, kv, cos, sin, pos, att, d_att, norm):
    rows, keys = qkv.shape[0], kv.shape[0]
    head_spec = pl.BlockSpec((rows, HEAD), lambda head: (0, head))
    return pl.pallas_call(
        backward_kernel,
        grid=(HEADS,),
        out_shape=(
            jax.ShapeDtypeStruct((rows, HEADS * HEAD), BF16),
            jax.ShapeDtypeStruct((keys, 2 * HEAD), F32),
        ),
        in_specs=[
            pl.BlockSpec(memory_space=pltpu.SMEM),
            head_spec,
            whole_spec((keys, 2 * HEAD)),
            whole_spec((rows, HEAD // 2)),
            whole_spec((rows, HEAD // 2)),
            whole_spec((rows, 1)),
            head_spec,
            head_spec,
            pl.BlockSpec((1, rows, 1), lambda head: (head, 0, 0)),
        ],
        out_specs=(head_spec, whole_spec((keys, 2 * HEAD))),
        compiler_params=pltpu.CompilerParams(
            dimension_semantics=("arbitrary",), vmem_limit_bytes=40 << 20
        ),
        cost_estimate=pl.CostEstimate(
            flops=10 * rows * keys * HEADS * HEAD,
            bytes_accessed=8 * rows * HEADS * HEAD + 12 * keys * HEAD,
            transcendentals=rows * keys * HEADS,
        ),
        name="attention_backward",
    )(first, qkv, kv, cos, sin, pos, att, d_att, norm)


def after(value, *earlier):
    return lax.optimization_barrier((value, *earlier))[0]


def row_scale(rows_b, axis=-1):
    rows = rows_b.astype(F32)
    return lax.rsqrt(jnp.mean(rows * rows, axis=axis, keepdims=True) + NORM_EPS)


def gelu_parts(value):
    root = math.sqrt(2.0 / math.pi)
    square = value * value
    tanh = jnp.tanh(root * (value + 0.044715 * value * square))
    cdf = 0.5 * (1.0 + tanh)
    slope = cdf + 0.5 * value * (1.0 - tanh * tanh) * root * (1.0 + 3 * 0.044715 * square)
    return value * cdf, slope


def scaled(weight, gain):
    return (weight.astype(F32) * gain.astype(F32)[:, None]).astype(BF16)


def on_device(
    inputs, positions, norm1_gain, qkv_weight, out_weight, norm2_gain, gate_weight,
    up_weight, down_weight, cotangent,
):
    me = lax.axis_index("mdl")
    size = lax.axis_size("mdl")
    head_cols = HEADS * HEAD
    width = inputs.shape[1]
    features = width * size

    def from_tok(weight, dim):
        return lax.all_gather(weight, "tok", axis=dim, tiled=True)

    def to_tok(grad, dim):
        total = lax.psum_scatter(grad, "tok", scatter_dimension=dim, tiled=True)
        return total.astype(F32)

    w_qkv = from_tok(scaled(qkv_weight, norm1_gain), 0)
    w_out = from_tok(out_weight, 1)
    w_gate = from_tok(scaled(gate_weight, norm2_gain), 0)
    w_up = from_tok(scaled(up_weight, norm2_gain), 0)
    w_down = from_tok(down_weight, 1)

    rows_in = gather_mdl(inputs, 1)
    scale_one = row_scale(rows_in)
    qkv_part = (nn(rows_in, w_qkv) * scale_one).astype(BF16)
    qkv = rows_to_cols(qkv_part)
    count = qkv.shape[0]
    half = HEAD // 2
    frequency = jnp.exp(jnp.arange(half, dtype=F32) * (-2.0 * math.log(10000.0) / HEAD))
    angles = positions.astype(F32)[:, None] * frequency[None, :]
    cos, sin = jnp.cos(angles), jnp.sin(angles)
    key_rows = turn(qkv[:, head_cols : head_cols + HEAD].astype(F32), cos, sin).astype(BF16)
    kv = gather_mdl(jnp.concatenate([key_rows, qkv[:, head_cols + HEAD :]], axis=1), 0)
    first = (me * count).astype(jnp.int32).reshape(1)
    pos = positions[:, None]
    attended, log_norm = attention_forward(first, qkv, kv, cos, sin, pos)
    head_block = cols_to_rows(attended)
    residual = inputs.astype(F32)
    mixed = residual + scatter_mdl(nn(head_block, w_out).astype(BF16), 1)

    rows_two = gather_mdl(mixed.astype(BF16), 1)
    scale_two = row_scale(rows_two)
    gate_in = nn(rows_two, w_gate) * scale_two
    up_in = nn(rows_two, w_up) * scale_two
    gelu, _ = gelu_parts(gate_in)
    hidden = (gelu * up_in).astype(BF16)
    gate_in, up_in, hidden = lax.optimization_barrier((gate_in, up_in, hidden))
    gelu, slope = gelu_parts(gate_in)

    down_local = tn(hidden, cotangent).astype(BF16)
    down_grad = to_tok(down_local, 1)
    d_hidden = nt(cotangent, w_down)
    d_gate = d_hidden * up_in * slope
    d_up = d_hidden * gelu
    stat_two = jnp.sum(d_gate * gate_in + d_up * up_in, axis=1)
    gate_scaled = (d_gate * scale_two).astype(BF16)
    up_scaled = (d_up * scale_two).astype(BF16)
    d_two_part = (nt(d_gate.astype(BF16), w_gate) + nt(d_up.astype(BF16), w_up)).astype(BF16)
    rows_later = after(rows_two, d_two_part)
    gate_local = tn(rows_later, gate_scaled).astype(BF16)
    gate_sum = to_tok(gate_local, 0)
    rows_later = after(rows_two, gate_local)
    up_local = tn(rows_later, up_scaled).astype(BF16)
    up_sum = to_tok(up_local, 0)
    d_two = scatter_mdl(d_two_part, 1)
    stat_two = sum_mdl(stat_two.reshape(8, -1)).reshape(-1, 1) * (1.0 / features)
    scale_mixed = scale_two * mixed
    cotangent_own = lax.dynamic_slice_in_dim(cotangent, me * width, width, 1).astype(F32)
    d_mixed = cotangent_own + scale_two * (d_two - scale_mixed * stat_two)

    d_mixed_b = after(d_mixed.astype(BF16), up_local)
    d_mixed_rows = gather_mdl(d_mixed_b, 1)
    hidden_later = after(hidden, d_mixed_b)
    ffn_part = nn(hidden_later, w_down).astype(BF16)
    d_head = nt(after(d_mixed_rows, ffn_part), w_out).astype(BF16)
    d_attended = rows_to_cols(d_head)
    out_local = tn(d_mixed_rows, after(head_block, d_head)).astype(BF16)
    out_grad = to_tok(out_local, 0).T
    d_attended = after(d_attended, out_local)
    block_out = (mixed + scatter_mdl(ffn_part, 1)).astype(BF16)
    d_query, d_kv = attention_backward(
        first, qkv, kv, cos, sin, pos, attended, d_attended, log_norm
    )
    d_kv = scatter_mdl(d_kv.astype(BF16), 0)
    d_key = unturn(d_kv[:, :HEAD], cos, sin).astype(BF16)
    d_qkv = jnp.concatenate([d_query, d_key, d_kv[:, HEAD:].astype(BF16)], axis=1)
    stat_one = jnp.sum(d_qkv.astype(F32) * qkv.astype(F32), axis=1)
    d_qkv_part = cols_to_rows(d_qkv)
    stat_rows = jnp.zeros((size, count), F32)
    stat_rows = sum_mdl(lax.dynamic_update_slice(stat_rows, stat_one[None], (me, 0)))
    stat_one = stat_rows.reshape(-1, 1) * (1.0 / features)
    qkv_local = tn(rows_in, (d_qkv_part.astype(F32) * scale_one).astype(BF16)).astype(BF16)
    qkv_sum = to_tok(qkv_local, 0)
    d_one = scatter_mdl(nt(d_qkv_part, w_qkv).astype(BF16), 1)
    input_grad = d_mixed + scale_one * (d_one - (scale_one * residual) * stat_one)

    norm1_late, norm2_late, qkv_late, gate_late, up_late, _ = lax.optimization_barrier(
        (norm1_gain, norm2_gain, qkv_weight, gate_weight, up_weight, up_local)
    )

    def unfold(total, gain):
        return total * gain.astype(F32)[:, None]

    def gain_grad(*pairs):
        return sum(jnp.sum(weight.astype(F32) * total, axis=1) for weight, total in pairs)

    gain_two_grad = sum_mdl(gain_grad((gate_late, gate_sum), (up_late, up_sum)))
    gain_one_grad = sum_mdl(gain_grad((qkv_late, qkv_sum)))
    return (
        block_out,
        input_grad,
        gain_one_grad,
        unfold(qkv_sum, norm1_late),
        out_grad,
        gain_two_grad,
        unfold(gate_sum, norm2_late),
        unfold(up_sum, norm2_late),
        down_grad,
    )


def solution(mesh):
    return jax.shard_map(
        on_device,
        mesh=mesh,
        in_specs=(
            P("tok", "mdl"),
            P(("tok", "mdl")),
            P("tok"),
            P("tok", "mdl"),
            P("mdl", "tok"),
            P("tok"),
            P("tok", "mdl"),
            P("tok", "mdl"),
            P("mdl", "tok"),
            P("tok", None),
        ),
        out_specs=(
            P("tok", "mdl"),
            P("tok", "mdl"),
            P("tok"),
            P("tok", "mdl"),
            P("mdl", "tok"),
            P("tok"),
            P("tok", "mdl"),
            P("tok", "mdl"),
            P("mdl", "tok"),
        ),
        check_vma=False,
    )
```

time: 1470 us -> 1110 us (0.76)
  waiting for transfers between devices: 914 us -> 652 us
  blocking collectives: 81.6 us -> 18.8 us
  local copies, waits for them, and re-layouts: 76.6 us -> 29.5 us
  other arithmetic: 102 us -> 62.7 us
  starting transfers between devices: 33 us -> 61 us
  Pallas kernels: 0 us -> 26.5 us
    ppermute x12 -> x44, waiting for transfers between devices: 5.73 us -> 290 us  [swap(): return lax.ppermute(block, 'mdl', [(i, i ^ distance) for i in range(size)])]
    psum x3 -> x0, waiting for transfers between devices: 256 us -> none  [the longest x1 117 us: on_device(): lax.psum(attn_part.astype(jnp.bfloat16), 'mdl').astype(jnp.float32)]
    all_gather x6 -> x5, waiting for transfers between devices: 309 us -> 78.2 us  [from_tok(): return lax.all_gather(weight, 'tok', axis=dim, tiled=True)]
    unnamed x2 -> x0, blocking collectives: 60.4 us -> none
    reduce_scatter x5, waiting for transfers between devices: 305 us -> 245 us  [to_tok(): total = lax.psum_scatter(grad, 'tok', scatter_dimension=dim, tiled=True)]
    reduce_sum x6 -> x3, other arithmetic: 38.5 us -> 2.67 us  [the longest x2 2.17 us: row_scale(): return lax.rsqrt(jnp.mean(rows * rows, axis=axis, keepdims=True) + NORM_EPS)]
    ppermute x12 -> x44, starting transfers between devices: 21.5 us -> 48.8 us  [swap(): return lax.ppermute(block, 'mdl', [(i, i ^ distance) for i in range(size)])]
    pallas_call x0 -> x2, Pallas kernels: none -> 26.5 us  [the longest x1 15.7 us: attention_backward(): pl.pallas_call(backward_kernel, grid=(HEADS,), out_shape=(jax.ShapeDtypeS...]
  transfers between devices with their start and end apart: 30 -> 57, of which waited for: 16 -> 32; matrix products, arithmetic and copies ran while one was open for 23% -> 19% of each run, Pallas kernels for 0% -> 1%
where the time goes in v1:
time: 1110 us; the launch traced here: 1100 us
  waiting for transfers between devices  652 us (59%)
  matrix products  231 us (21%)
  other arithmetic  62.7 us (6%)
  starting transfers between devices  61 us (5%)
  local copies, waits for them, and re-layouts  29.5 us (3%)
  Pallas kernels  26.5 us (2%)
  blocking collectives  18.8 us (2%)
  between operations  15.7 us (1%)
    ppermute x44, waiting for transfers between devices, swap(): return lax.ppermute(block, 'mdl', [(i, i ^ distance) for i in range(size)])  290 us
    reduce_scatter x5, waiting for transfers between devices, to_tok(): total = lax.psum_scatter(grad, 'tok', scatter_dimension=dim, tiled=True)  245 us
    dot_general x5, matrix products, tn(): lax.dot_general(left_op, right_op, (((0,), (0,)), ((), ())), preferred_el...  81.7 us
    dot_general x5, matrix products, nt(): lax.dot_general(left_op, right_op, (((1,), (1,)), ((), ())), preferred_el...  79.7 us
    all_gather x5, waiting for transfers between devices, from_tok(): return lax.all_gather(weight, 'tok', axis=dim, tiled=True)  78.2 us
    dot_general x5, matrix products, nn(): return jnp.dot(left_op, right_op, preferred_element_type=F32)  69.6 us
    ppermute x44, starting transfers between devices, swap(): return lax.ppermute(block, 'mdl', [(i, i ^ distance) for i in range(size)])  48.8 us
    all_to_all x2, waiting for transfers between devices, rows_to_cols(): return lax.all_to_all(block, 'mdl', split_axis=0, concat_axis=1, tiled=True)  22.3 us
  transfers between devices with their start and end apart: 57, of which 32 were waited for; matrix products, arithmetic and copies ran while one was open for 19% of the time, Pallas kernels for 1%

profile of v1, /device:TPU:0, one launch (start us, length us, event | category | flops | bytes accessed | tf_op | source)
XLA Modules:
  0.0 1097.2 jit_solution(577114914185097247)
XLA Ops:
  11.4 3.7 multiply_convert_fusion.7
  15.7 3.0 collective-permute-start
  20.3 27.3 %collective-permute-done = bf16[1024,640]{1,0:T(8,128)(2,1)S(1)} collective-permute-done((bf16[1024,640]{1,0:T(8,128)(2,1)S(1)}, bf16[1024,640]{1,0:T(8,128)(2,1)S(1)}, u32[]{:S(2)}, u32[]{:S(2)}) %collective-permute-start) | collective-permute-done | bytes 1310752 | tf_op jit(solution)/shard_map/ppermute | solution.py:37
  55.6 9.0 collective-permute-done.2
  64.8 3.2 collective-permute-done.3
  72.6 9.1 multiply_convert_fusion.6
  81.7 3.6 all-to-all-start
  85.3 17.5 %all-to-all-done = bf16[4,256,768]{2,1,0:T(8,128)(2,1)S(1)} async-done(((bf16[4,256,768]{2,1,0:T(8,128)(2,1)}), bf16[4,256,768]{2,1,0:T(8,128)(2,1)S(1)}, u32[]{:S(2)}, u32[]{:S(2)}) %all-to-all-start) | async-done | bytes 1572896 | tf_op jit(solution)/shard_map/all_to_all | solution.py:111
  107.6 5.3 collective-permute-done.4
  113.6 2.4 collective-permute-start.7
  118.9 10.8 attention_forward.1
  132.4 4.0 all-to-all-start.1
  136.4 13.3 %all-to-all-done.1 = bf16[256,4,640]{2,0,1:T(8,128)(2,1)S(1)} async-done(((bf16[256,4,640]{2,0,1:T(8,128)(2,1)}), bf16[256,4,640]{2,0,1:T(8,128)(2,1)S(1)}, u32[]{:S(2)}, u32[]{:S(2)}) %all-to-all-start.1) | async-done | bytes 1310752 | tf_op jit(solution)/shard_map/all_to_all | solution.py:115
  149.7 6.9 convolution_convert_fusion.4
  159.3 27.7 %collective-permute-done.8 = bf16[2,512,640]{2,1,0:T(8,128)(2,1)S(1)} collective-permute-done((bf16[2,512,640]{2,1,0:T(8,128)(2,1)S(1)}, bf16[2,512,640]{2,1,0:T(8,128)(2,1)S(1)}, u32[]{:S(2)}, u32[]{:S(2)}) %collective-permute-start.8) | collective-permute-done | bytes 1310752 | tf_op jit(solution)/shard_map/ppermute | solution.py:37
  187.3 15.0 %collective-permute-done.9 = bf16[512,640]{1,0:T(8,128)(2,1)S(1)} collective-permute-done((bf16[512,640]{1,0:T(8,128)(2,1)S(1)}, bf16[512,640]{1,0:T(8,128)(2,1)S(1)}, u32[]{:S(2)}, u32[]{:S(2)}) %collective-permute-start.9) | collective-permute-done | bytes 655392 | tf_op jit(solution)/shard_map/ppermute | solution.py:37
  203.4 13.6 %collective-permute-done.11 = bf16[512,640]{1,0:T(8,128)(2,1)S(1)} collective-permute-done((bf16[512,640]{1,0:T(8,128)(2,1)S(1)}, bf16[512,640]{1,0:T(8,128)(2,1)S(1)}, u32[]{:S(2)}, u32[]{:S(2)}) %collective-permute-start.11) | collective-permute-done | bytes 655392 | tf_op jit(solution)/shard_map/ppermute | solution.py:37
  220.0 25.9 %collective-permute-done.12 = bf16[1024,640]{1,0:T(8,128)(2,1)S(1)} collective-permute-done((bf16[1024,640]{1,0:T(8,128)(2,1)S(1)}, bf16[1024,640]{1,0:T(8,128)(2,1)S(1)}, u32[]{:S(2)}, u32[]{:S(2)}) %collective-permute-start.12) | collective-permute-done | bytes 1310752 | tf_op jit(solution)/shard_map/ppermute | solution.py:37
  246.8 2.4 collective-permute-done.13
  249.9 11.1 %collective-permute-done.14 = bf16[512,640]{1,0:T(8,128)(2,1)S(1)} collective-permute-done((bf16[512,640]{1,0:T(8,128)(2,1)S(1)}, bf16[512,640]{1,0:T(8,128)(2,1)S(1)}, u32[]{:S(2)}, u32[]{:S(2)}) %collective-permute-start.14) | collective-permute-done | bytes 655392 | tf_op jit(solution)/shard_map/ppermute | solution.py:37
  261.2 2.3 copy-done.23
  264.6 17.2 %convolution_multiply_fusion.1 = f32[1024,1920]{1,0:T(8,128)} fusion(bf16[1024,2560]{1,0:T(8,128)(2,1)} %copy-done.23, bf16[2560,1920]{1,0:T(8,128)(2,1)} %all-gather.10.cloned.1.call-done, f32[1024]{0:T(1024)S(1)} %add_rsqrt_fusion), kind=kOutput, calls=%fused_computation.21 | convolution fusion | flops 10068295680 | bytes 22941696 | tf_op jit(solution)/shard_map/dot_general | solution.py:32
  281.8 5.2 all-gather.12.cloned.1.call-done
  287.0 20.9 %multiply_convert_fusion.2 = (bf16[1024,1920]{1,0:T(8,128)(2,1)}, f32[1024,1920]{1,0:T(8,128)}) fusion(f32[1024,1920]{1,0:T(8,128)} %convolution_multiply_fusion.1, f32[1024]{0:T(1024)S(1)} %add_rsqrt_fusion, bf16[1024,2560]{1,0:T(8,128)(2,1)} %copy-done.23, bf16[2560,1920]{1,0:T(8,128)(2,1)} %all-gather.12.cloned.1.call-done), kind=kOutput, calls=%fused_computation.14 | convolution fusion | flops 10087956480 | bytes 34738176 | tf_op jit(solution)/shard_map/dot_general | solution.py:32
  307.9 73.0 %all-gather.14.cloned.1.call-done = bf16[1920,2560]{0,1:T(8,128)(2,1)} async-done(((bf16[1920,320]{0,1:T(8,128)(2,1)}), bf16[1920,2560]{0,1:T(8,128)(2,1)}) %all-gather.14.cloned.1.call-update) | async-done | bytes 9830416 | tf_op jit(solution)/shard_map/all_gather | solution.py:277
  380.9 23.1 %add_reduce_fusion = (f32[1024]{0:T(1024)S(1)}, f32[1024,1920]{1,0:T(8,128)}) fusion(f32[1024,1920]{1,0:T(8,128)} %get-tuple-element.30, f32[1024,1920]{1,0:T(8,128)} %convolution_multiply_fusion.1, bf16[1024,2560]{1,0:T(8,128)(2,1)} %param.19, bf16[1920,2560]{0,1:T(8,128)(2,1)} %all-gather.14.cloned.1.call-done), kind=kOutput, calls=%fused_computation.8 | convolution fusion | flops 10113514496 | bytes 38670336 | tf_op jit(solution)/shard_map/dot_general | solution.py:20
  403.9 22.3 %fusion.1 = f32[1024,2560]{1,0:T(8,128)} fusion(bf16[2560,1920]{1,0:T(8,128)(2,1)} %all-gather.10.cloned.1.call-done, f32[1024,1920]{1,0:T(8,128)} %convolution_multiply_fusion.1, f32[1024,1920]{1,0:T(8,128)} %get-tuple-element.106, f32[1024,1920]{1,0:T(8,128)} %get-tuple-element.30), kind=kOutput, calls=%fused_computation.23 | convolution fusion | flops 10103685120 | bytes 43909120 | tf_op jit(solution)/shard_map/dot_general | solution.py:20
  426.3 24.5 %add_convert_fusion = bf16[1024,2560]{1,0:T(8,128)(2,1)} fusion(f32[1024,2560]{1,0:T(8,128)} %fusion.1, bf16[2560,1920]{1,0:T(8,128)(2,1)} %all-gather.12.cloned.1.call-done, f32[1024,1920]{1,0:T(8,128)} %get-tuple-element.106, f32[1024,1920]{1,0:T(8,128)} %convolution_multiply_fusion.1), kind=kOutput, calls=%fused_computation.3 | convolution fusion | flops 10091233280 | bytes 41287680 | tf_op jit(solution)/shard_map/dot_general | solution.py:20
  456.6 27.3 %collective-permute-done.16 = bf16[2,512,640]{2,1,0:T(8,128)(2,1)S(1)} collective-permute-done((bf16[2,512,640]{2,1,0:T(8,128)(2,1)S(1)}, bf16[2,512,640]{2,1,0:T(8,128)(2,1)S(1)}, u32[]{:S(2)}, u32[]{:S(2)}) %collective-permute-start.16) | collective-permute-done | bytes 1310752 | tf_op jit(solution)/shard_map/ppermute | solution.py:37
  487.7 24.3 %convolution_convert_fusion.2 = bf16[2560,1920]{1,0:T(8,128)(2,1)} fusion(bf16[1024,2560]{1,0:T(8,128)(2,1)} %copy-done.23, f32[1024]{0:T(1024)S(1)} %add_rsqrt_fusion, f32[1024,1920]{1,0:T(8,128)} %convolution_multiply_fusion.1, f32[1024,1920]{1,0:T(8,128)} %get-tuple-element.106, f32[1024,1920]{1,0:T(8,128)} %get-tuple-element.30), kind=kOutput, calls=%fused_computation.2 | convolution fusion | flops 10110566400 | bytes 38670336 | tf_op jit(solution)/shard_map/dot_general | solution.py:26
  512.7 3.5 fusion.26
  517.6 22.8 %convolution_convert_fusion.1 = bf16[2560,1920]{1,0:T(8,128)(2,1)} fusion(bf16[1024,2560]{1,0:T(8,128)(2,1)} %copy-done.23, f32[1024]{0:T(1024)S(1)} %add_rsqrt_fusion, f32[1024,1920]{1,0:T(8,128)} %get-tuple-element.106, f32[1024,1920]{1,0:T(8,128)} %convolution_multiply_fusion.1), kind=kOutput, calls=%fused_computation.1 | convolution fusion | flops 10092871680 | bytes 30806016 | tf_op jit(solution)/shard_map/dot_general | solution.py:26
  542.8 4.5 fusion.57
  549.3 27.2 %collective-permute-done.26 = bf16[1024,640]{1,0:T(8,128)(2,1)S(1)} collective-permute-done((bf16[1024,640]{1,0:T(8,128)(2,1)S(1)}, bf16[1024,640]{1,0:T(8,128)(2,1)S(1)}, u32[]{:S(2)}, u32[]{:S(2)}) %collective-permute-start.26) | collective-permute-done | bytes 1310752 | tf_op jit(solution)/shard_map/ppermute | solution.py:37
  579.2 15.5 %convolution_convert_fusion.3 = bf16[1024,2560]{1,0:T(8,128)(2,1)} fusion(bf16[1024,1920]{1,0:T(8,128)(2,1)S(1)} %copy-done.50, bf16[1920,2560]{0,1:T(8,128)(2,1)} %all-gather.14.cloned.1.call-done), kind=kOutput, calls=%fused_computation.15 | convolution fusion | flops 10068951040 | bytes 19005440 | tf_op jit(solution)/shard_map/dot_general | solution.py:32
  597.2 5.3 convolution_convert_fusion.8
  602.5 4.3 all-to-all-start.2
  606.9 9.0 convolution_convert_fusion.7
  615.9 4.8 all-to-all-done.2
  624.7 15.7 %attention_backward.1 = (bf16[256,2560]{1,0:T(8,128)(2,1)S(1)}, f32[1024,512]{1,0:T(8,128)S(1)}) custom-call(s32[1]{0:T(128)} %bitcast.first_ref, bf16[256,3072]{1,0:T(8,128)(2,1)S(1)} %bitcast.206, bf16[1024,512]{1,0:T(8,128)(2,1)S(1)} %copy-done.5, f32[256,128]{1,0:T(8,128)S(1)} %copy-done.11, f32[256,128]{1,0:T(8,128)S(1)} %copy-done.9, ...), custom_call_target="tpu_custom_call" | custom-call | flops 6710886400 | bytes 8388608 | tf_op jit(solution)/shard_map/attention_backward/pallas_call | solution.py:213
  643.7 5.2 collective-permute-done.30
  649.6 4.4 collective-permute-done.31
  654.7 4.5 collective-permute-done.33
  660.1 18.8 %all_to_all.76 = bf16[256,4,768]{2,0,1:T(8,128)(2,1)S(1)} all-to-all(bf16[256,4,768]{2,0,1:T(8,128)(2,1)S(1)} %bitcast.212), channel_id=1, replica_groups=mesh['tok'=8,'mdl'=4] {'mdl'}, dimensions={1} | all-to-all | bytes 3145728 | tf_op jit(solution)/shard_map/all_to_all | solution.py:115
  678.9 9.0 convolution_convert_fusion.6
  690.2 16.7 %convolution_convert_fusion = bf16[1920,2560]{0,1:T(8,128)(2,1)} fusion(bf16[1024,1920]{1,0:T(8,128)(2,1)} %get-tuple-element.35, bf16[1024,2560]{1,0:T(8,128)(2,1)} %param.19), kind=kOutput, calls=%fused_computation | convolution fusion | flops 10071244800 | bytes 19005440 | tf_op jit(solution)/shard_map/dot_general | solution.py:26
  710.4 4.5 convolution_convert_fusion.5
  720.9 20.0 %collective-permute-done.22 = bf16[2,512,640]{2,1,0:T(8,128)(2,1)S(1)} collective-permute-done((bf16[2,512,640]{2,1,0:T(8,128)(2,1)S(1)}, bf16[2,512,640]{2,1,0:T(8,128)(2,1)S(1)}, u32[]{:S(2)}, u32[]{:S(2)}) %collective-permute-start.22) | collective-permute-done | bytes 1310752 | tf_op jit(solution)/shard_map/ppermute | solution.py:37
  740.9 2.6 fusion.21
  744.6 18.0 %collective-permute-done.34 = bf16[2,512,640]{2,1,0:T(8,128)(2,1)S(1)} collective-permute-done((bf16[2,512,640]{2,1,0:T(8,128)(2,1)S(1)}, bf16[2,512,640]{2,1,0:T(8,128)(2,1)S(1)}, u32[]{:S(2)}, u32[]{:S(2)}) %collective-permute-start.34) | collective-permute-done | bytes 1310752 | tf_op jit(solution)/shard_map/ppermute | solution.py:37
  765.1 26.7 %collective-permute-done.23 = bf16[512,640]{1,0:T(8,128)(2,1)} collective-permute-done((bf16[512,640]{1,0:T(8,128)(2,1)}, bf16[512,640]{1,0:T(8,128)(2,1)}, u32[]{:S(2)}, u32[]{:S(2)}) %collective-permute-start.23) | collective-permute-done | bytes 655392 | tf_op jit(solution)/shard_map/ppermute | solution.py:37
  791.8 3.6 fusion.22
  799.2 3.4 fusion.18
  803.6 9.2 collective-permute-done.38
  814.1 2.8 fusion.20
  817.0 2.8 collective-permute-done.37
  819.8 2.6 fusion.16
  825.5 10.6 reduce-scatter.12.cloned.1.call-done
  836.1 103.9 %reduce-scatter.10.cloned.1.call-done = bf16[320,1920]{1,0:T(8,128)(2,1)} async-done(((bf16[2560,1920]{1,0:T(8,128)(2,1)}), bf16[320,1920]{1,0:T(8,128)(2,1)}) %reduce-scatter.10.cloned.1.call-update) | async-done | bytes 1228816 | tf_op jit(solution)/shard_map/reduce_scatter | solution.py:280
  940.1 5.4 convert_multiply_fusion.1
  947.0 4.5 fusion.8
  953.6 28.6 %reduce-scatter.8.cloned.1.call-done = bf16[320,640]{1,0:T(8,128)(2,1)} async-done(((bf16[2560,640]{1,0:T(8,128)(2,1)}), bf16[320,640]{1,0:T(8,128)(2,1)}) %reduce-scatter.8.cloned.1.call-update) | async-done | bytes 409616 | tf_op jit(solution)/shard_map/reduce_scatter | solution.py:280
  984.7 101.7 %reduce-scatter.14.cloned.1.call-done = bf16[1920,320]{0,1:T(8,128)(2,1)} async-done(((bf16[1920,2560]{0,1:T(8,128)(2,1)}), bf16[1920,320]{0,1:T(8,128)(2,1)}) %reduce-scatter.14.cloned.1.call-update) | async-done | bytes 1228816 | tf_op jit(solution)/shard_map/reduce_scatter | solution.py:280
  1086.4 2.9 convert_element_type.515
  (285 shorter events, 101.9 us)
Async XLA Ops:
  7.2 65.4 %all-gather.6.cloned.1.call-start = ((), (), s32[]{:S(2)}) async-start(), calls=%async_computation.9 | async-start | bytes 4423680 | tf_op jit(solution)/shard_map/all_gather | solution.py:277
  9.9 126.5 %all-gather.8.cloned.1.call-start = ((), (), s32[]{:S(2)}) async-start(), calls=%async_computation.10 | async-start | bytes 3686400 | tf_op jit(solution)/shard_map/all_gather | solution.py:277
  10.6 254.0 %all-gather.10.cloned.1.call-start = ((), (), s32[]{:S(2)}) async-start(), calls=%async_computation.11 | async-start | bytes 11059200 | tf_op jit(solution)/shard_map/all_gather | solution.py:277
  15.1 271.9 %all-gather.12.cloned.1.call-start = ((), (), s32[]{:S(2)}) async-start(), calls=%async_computation.12 | async-start | bytes 11059200 | tf_op jit(solution)/shard_map/all_gather | solution.py:277
  15.7 365.2 %all-gather.14.cloned.1.call-start = ((), (), s32[]{:S(2)}) async-start(), calls=%async_computation.13 | async-start | bytes 11059200 | tf_op jit(solution)/shard_map/all_gather | solution.py:277
  15.7 31.8 %collective-permute-start = (bf16[1024,640]{1,0:T(8,128)(2,1)S(1)}, bf16[1024,640]{1,0:T(8,128)(2,1)S(1)}, u32[]{:S(2)}, u32[]{:S(2)}) collective-permute-start(bf16[1024,640]{1,0:T(8,128)(2,1)S(1)} %copy-done.14), channel_id=1, source_target_pairs={{0,1},{1,0},{2,3},{3,2},{4,5},{5,4},{6,7},{7,6},{8,9},{9,8},{10,11... | collective-permute-start | bytes 3932168 | tf_op jit(solution)/shard_map/ppermute | solution.py:37
  18.8 31.4 %collective-permute-start.1 = (bf16[1024,640]{1,0:T(8,128)(2,1)S(1)}, bf16[1024,640]{1,0:T(8,128)(2,1)S(1)}, u32[]{:S(2)}, u32[]{:S(2)}) collective-permute-start(bf16[1024,640]{1,0:T(8,128)(2,1)S(1)} %copy-done.14), channel_id=1, source_target_pairs={{0,2},{1,3},{2,0},{3,1},{4,6},{5,7},{6,4},{7,5},{8,10},{9,11},{10,... | collective-permute-start | bytes 3932168 | tf_op jit(solution)/shard_map/ppermute | solution.py:37
  48.4 16.2 %collective-permute-start.2 = (bf16[512,640]{1,0:T(8,128)(2,1)}, bf16[512,640]{1,0:T(8,128)(2,1)S(1)}, u32[]{:S(2)}, u32[]{:S(2)}) collective-permute-start(bf16[512,640]{1,0:T(8,128)(2,1)} %slice.144), channel_id=1, source_target_pairs={{0,2},{1,3},{2,0},{3,1},{4,6},{5,7},{6,4},{7,5},{8,10},{9,11},{10,... | collective-permute-start | bytes 1966088 | tf_op jit(solution)/shard_map/ppermute | solution.py:37
  52.2 15.8 %collective-permute-start.3 = (bf16[512,640]{1,0:T(8,128)(2,1)}, bf16[512,640]{1,0:T(8,128)(2,1)}, u32[]{:S(2)}, u32[]{:S(2)}) collective-permute-start(bf16[512,640]{1,0:T(8,128)(2,1)} %slice.145), channel_id=1, source_target_pairs={{0,1},{1,0},{2,3},{3,2},{4,5},{5,4},{6,7},{7,6},{8,9},{9,8},{10,11... | collective-permute-start | bytes 1966088 | tf_op jit(solution)/shard_map/ppermute | solution.py:37
  81.7 21.2 %all-to-all-start = ((bf16[4,256,768]{2,1,0:T(8,128)(2,1)}), bf16[4,256,768]{2,1,0:T(8,128)(2,1)S(1)}, u32[]{:S(2)}, u32[]{:S(2)}) async-start(bf16[4,256,768]{2,1,0:T(8,128)(2,1)} %bitcast.1), calls=%async_computation | async-start | bytes 3145728 | tf_op jit(solution)/shard_map/all_to_all | solution.py:111
  105.4 7.5 collective-permute-start.4
  106.9 6.7 collective-permute-start.5
  112.9 5.0 collective-permute-start.6
  113.6 5.3 collective-permute-start.7
  132.4 17.4 %all-to-all-start.1 = ((bf16[256,4,640]{2,0,1:T(8,128)(2,1)}), bf16[256,4,640]{2,0,1:T(8,128)(2,1)S(1)}, u32[]{:S(2)}, u32[]{:S(2)}) async-start(bf16[256,4,640]{2,0,1:T(8,128)(2,1)} %bitcast.203), calls=%async_computation.1 | async-start | bytes 2621440 | tf_op jit(solution)/shard_map/all_to_all | solution.py:115
  157.0 30.0 %collective-permute-start.8 = (bf16[2,512,640]{2,1,0:T(8,128)(2,1)S(1)}, bf16[2,512,640]{2,1,0:T(8,128)(2,1)S(1)}, u32[]{:S(2)}, u32[]{:S(2)}) collective-permute-start(bf16[2,512,640]{2,1,0:T(8,128)(2,1)S(1)} %pad_maximum_fusion.1), channel_id=1, source_target_pairs={{0,1},{1,0},{2,3},{3,2},{4,5},{5,4},{6,7},{7,6},{8,9},{9,8},{10,11... | collective-permute-start | bytes 3932168 | tf_op jit(solution)/shard_map/ppermute | solution.py:37
  158.7 28.6 %collective-permute-start.10 = (bf16[2,512,640]{2,1,0:T(8,128)(2,1)S(1)}, bf16[2,512,640]{2,1,0:T(8,128)(2,1)S(1)}, u32[]{:S(2)}, u32[]{:S(2)}) collective-permute-start(bf16[2,512,640]{2,1,0:T(8,128)(2,1)S(1)} %pad_maximum_fusion.2), channel_id=1, source_target_pairs={{0,2},{1,3},{2,0},{3,1},{4,6},{5,7},{6,4},{7,5},{8,10},{9,11},{10,... | collective-permute-start | bytes 3932168 | tf_op jit(solution)/shard_map/ppermute | solution.py:37
  187.1 15.2 %collective-permute-start.9 = (bf16[512,640]{1,0:T(8,128)(2,1)S(1)}, bf16[512,640]{1,0:T(8,128)(2,1)S(1)}, u32[]{:S(2)}, u32[]{:S(2)}) collective-permute-start(bf16[512,640]{1,0:T(8,128)(2,1)S(1)} %fusion.29), channel_id=1, source_target_pairs={{0,2},{1,3},{2,0},{3,1},{4,6},{5,7},{6,4},{7,5},{8,10},{9,11},{10,... | collective-permute-start | bytes 1966088 | tf_op jit(solution)/shard_map/ppermute | solution.py:37
  202.7 14.3 %collective-permute-start.11 = (bf16[512,640]{1,0:T(8,128)(2,1)S(1)}, bf16[512,640]{1,0:T(8,128)(2,1)S(1)}, u32[]{:S(2)}, u32[]{:S(2)}) collective-permute-start(bf16[512,640]{1,0:T(8,128)(2,1)S(1)} %get-tuple-element.70), channel_id=1, source_target_pairs={{0,1},{1,0},{2,3},{3,2},{4,5},{5,4},{6,7},{7,6},{8,9},{9,8},{10,11... | collective-permute-start | bytes 1966088 | tf_op jit(solution)/shard_map/ppermute | solution.py:37
  218.3 27.5 %collective-permute-start.12 = (bf16[1024,640]{1,0:T(8,128)(2,1)S(1)}, bf16[1024,640]{1,0:T(8,128)(2,1)S(1)}, u32[]{:S(2)}, u32[]{:S(2)}) collective-permute-start(bf16[1024,640]{1,0:T(8,128)(2,1)S(1)} %get-tuple-element.50), channel_id=1, source_target_pairs={{0,1},{1,0},{2,3},{3,2},{4,5},{5,4},{6,7},{7,6},{8,9},{9,8},{10,11... | collective-permute-start | bytes 3932168 | tf_op jit(solution)/shard_map/ppermute | solution.py:37
  219.3 29.9 %collective-permute-start.13 = (bf16[1024,640]{1,0:T(8,128)(2,1)S(1)}, bf16[1024,640]{1,0:T(8,128)(2,1)S(1)}, u32[]{:S(2)}, u32[]{:S(2)}) collective-permute-start(bf16[1024,640]{1,0:T(8,128)(2,1)S(1)} %get-tuple-element.50), channel_id=1, source_target_pairs={{0,2},{1,3},{2,0},{3,1},{4,6},{5,7},{6,4},{7,5},{8,10},{9,11},{10,... | collective-permute-start | bytes 3932168 | tf_op jit(solution)/shard_map/ppermute | solution.py:37
  245.9 15.1 %collective-permute-start.14 = (bf16[512,640]{1,0:T(8,128)(2,1)S(1)}, bf16[512,640]{1,0:T(8,128)(2,1)S(1)}, u32[]{:S(2)}, u32[]{:S(2)}) collective-permute-start(bf16[512,640]{1,0:T(8,128)(2,1)S(1)} %slice.156), channel_id=1, source_target_pairs={{0,2},{1,3},{2,0},{3,1},{4,6},{5,7},{6,4},{7,5},{8,10},{9,11},{10,... | collective-permute-start | bytes 1966088 | tf_op jit(solution)/shard_map/ppermute | solution.py:37
  249.3 11.8 %collective-permute-start.15 = (bf16[512,640]{1,0:T(8,128)(2,1)S(1)}, bf16[512,640]{1,0:T(8,128)(2,1)S(1)}, u32[]{:S(2)}, u32[]{:S(2)}) collective-permute-start(bf16[512,640]{1,0:T(8,128)(2,1)S(1)} %slice.157), channel_id=1, source_target_pairs={{0,1},{1,0},{2,3},{3,2},{4,5},{5,4},{6,7},{7,6},{8,9},{9,8},{10,11... | collective-permute-start | bytes 1966088 | tf_op jit(solution)/shard_map/ppermute | solution.py:37
  452.9 31.0 %collective-permute-start.16 = (bf16[2,512,640]{2,1,0:T(8,128)(2,1)S(1)}, bf16[2,512,640]{2,1,0:T(8,128)(2,1)S(1)}, u32[]{:S(2)}, u32[]{:S(2)}) collective-permute-start(bf16[2,512,640]{2,1,0:T(8,128)(2,1)S(1)} %pad_maximum_fusion.3), channel_id=1, source_target_pairs={{0,1},{1,0},{2,3},{3,2},{4,5},{5,4},{6,7},{7,6},{8,9},{9,8},{10,11... | collective-permute-start | bytes 3932168 | tf_op jit(solution)/shard_map/ppermute | solution.py:37
  454.4 57.6 %collective-permute-start.20 = (f32[8,128]{1,0:T(8,128)S(1)}, f32[8,128]{1,0:T(8,128)S(1)}, u32[]{:S(2)}, u32[]{:S(2)}) collective-permute-start(f32[8,128]{1,0:T(8,128)S(1)} %bitcast.218), channel_id=1, source_target_pairs={{0,1},{1,0},{2,3},{3,2},{4,5},{5,4},{6,7},{7,6},{8,9},{9,8},{10,11... | collective-permute-start | bytes 12296 | tf_op jit(solution)/shard_map/ppermute | solution.py:37
  455.1 57.6 %collective-permute-start.18 = (bf16[2,512,640]{2,1,0:T(8,128)(2,1)S(1)}, bf16[2,512,640]{2,1,0:T(8,128)(2,1)}, u32[]{:S(2)}, u32[]{:S(2)}) collective-permute-start(bf16[2,512,640]{2,1,0:T(8,128)(2,1)S(1)} %pad_maximum_fusion.4), channel_id=1, source_target_pairs={{0,2},{1,3},{2,0},{3,1},{4,6},{5,7},{6,4},{7,5},{8,10},{9,11},{10,... | collective-permute-start | bytes 3932168 | tf_op jit(solution)/shard_map/ppermute | solution.py:37
  486.2 26.5 %collective-permute-start.17 = (bf16[512,640]{1,0:T(8,128)(2,1)S(1)}, bf16[512,640]{1,0:T(8,128)(2,1)}, u32[]{:S(2)}, u32[]{:S(2)}) collective-permute-start(bf16[512,640]{1,0:T(8,128)(2,1)S(1)} %fusion.25), channel_id=1, source_target_pairs={{0,2},{1,3},{2,0},{3,1},{4,6},{5,7},{6,4},{7,5},{8,10},{9,11},{10,... | collective-permute-start | bytes 1966088 | tf_op jit(solution)/shard_map/ppermute | solution.py:37
  512.0 28.4 %collective-permute-start.21 = (f32[8,128]{1,0:T(8,128)S(1)}, f32[8,128]{1,0:T(8,128)}, u32[]{:S(2)}, u32[]{:S(2)}) collective-permute-start(f32[8,128]{1,0:T(8,128)S(1)} %bitcast_add_fusion), channel_id=1, source_target_pairs={{0,2},{1,3},{2,0},{3,1},{4,6},{5,7},{6,4},{7,5},{8,10},{9,11},{10,... | collective-permute-start | bytes 12296 | tf_op jit(solution)/shard_map/ppermute | solution.py:37
  516.2 25.1 %collective-permute-start.19 = (bf16[512,640]{1,0:T(8,128)(2,1)}, bf16[512,640]{1,0:T(8,128)(2,1)S(1)}, u32[]{:S(2)}, u32[]{:S(2)}) collective-permute-start(bf16[512,640]{1,0:T(8,128)(2,1)} %get-tuple-element.64), channel_id=1, source_target_pairs={{0,1},{1,0},{2,3},{3,2},{4,5},{5,4},{6,7},{7,6},{8,9},{9,8},{10,11... | collective-permute-start | bytes 1966088 | tf_op jit(solution)/shard_map/ppermute | solution.py:37
  542.8 36.4 %copy-start.50 = (bf16[1024,1920]{1,0:T(8,128)(2,1)S(1)}, bf16[1024,1920]{1,0:T(8,128)(2,1)}, u32[]{:S(2)}) copy-start(bf16[1024,1920]{1,0:T(8,128)(2,1)} %get-tuple-element.35) | copy-start | bytes 11796484
  547.3 29.3 %collective-permute-start.26 = (bf16[1024,640]{1,0:T(8,128)(2,1)S(1)}, bf16[1024,640]{1,0:T(8,128)(2,1)S(1)}, u32[]{:S(2)}, u32[]{:S(2)}) collective-permute-start(bf16[1024,640]{1,0:T(8,128)(2,1)S(1)} %get-tuple-element.34), channel_id=1, source_target_pairs={{0,1},{1,0},{2,3},{3,2},{4,5},{5,4},{6,7},{7,6},{8,9},{9,8},{10,11... | collective-permute-start | bytes 3932168 | tf_op jit(solution)/shard_map/ppermute | solution.py:37
  547.9 30.3 %collective-permute-start.27 = (bf16[1024,640]{1,0:T(8,128)(2,1)S(1)}, bf16[1024,640]{1,0:T(8,128)(2,1)S(1)}, u32[]{:S(2)}, u32[]{:S(2)}) collective-permute-start(bf16[1024,640]{1,0:T(8,128)(2,1)S(1)} %get-tuple-element.34), channel_id=1, source_target_pairs={{0,2},{1,3},{2,0},{3,1},{4,6},{5,7},{6,4},{7,5},{8,10},{9,11},{10,... | collective-permute-start | bytes 3932168 | tf_op jit(solution)/shard_map/ppermute | solution.py:37
  576.7 19.1 %collective-permute-start.28 = (bf16[512,640]{1,0:T(8,128)(2,1)S(1)}, bf16[512,640]{1,0:T(8,128)(2,1)S(1)}, u32[]{:S(2)}, u32[]{:S(2)}) collective-permute-start(bf16[512,640]{1,0:T(8,128)(2,1)S(1)} %slice.166), channel_id=1, source_target_pairs={{0,2},{1,3},{2,0},{3,1},{4,6},{5,7},{6,4},{7,5},{8,10},{9,11},{10,... | collective-permute-start | bytes 1966088 | tf_op jit(solution)/shard_map/ppermute | solution.py:37
  578.3 17.6 %collective-permute-start.29 = (bf16[512,640]{1,0:T(8,128)(2,1)S(1)}, bf16[512,640]{1,0:T(8,128)(2,1)S(1)}, u32[]{:S(2)}, u32[]{:S(2)}) collective-permute-start(bf16[512,640]{1,0:T(8,128)(2,1)S(1)} %slice.167), channel_id=1, source_target_pairs={{0,1},{1,0},{2,3},{3,2},{4,5},{5,4},{6,7},{7,6},{8,9},{9,8},{10,11... | collective-permute-start | bytes 1966088 | tf_op jit(solution)/shard_map/ppermute | solution.py:37
  602.5 18.2 %all-to-all-start.2 = ((bf16[4,256,640]{2,1,0:T(8,128)(2,1)}), bf16[4,256,640]{2,1,0:T(8,128)(2,1)}, u32[]{:S(2)}, u32[]{:S(2)}) async-start(bf16[4,256,640]{2,1,0:T(8,128)(2,1)} %bitcast.32), calls=%async_computation.2 | async-start | bytes 2621440 | tf_op jit(solution)/shard_map/all_to_all | solution.py:111
  606.8 215.5 %reduce-scatter.6.cloned.1.call-start = ((), (), s32[]{:S(2)}) async-start(), calls=%async_computation.14 | async-start | bytes 4423680 | tf_op jit(solution)/shard_map/reduce_scatter | solution.py:280
  641.6 7.3 collective-permute-start.30
  643.1 6.5 collective-permute-start.32
  649.0 5.0 collective-permute-start.31
  654.1 5.0 collective-permute-start.33
  687.9 148.2 %reduce-scatter.12.cloned.1.call-start = ((), (), s32[]{:S(2)}) async-start(), calls=%async_computation.17 | async-start | bytes 11059200 | tf_op jit(solution)/shard_map/reduce_scatter | solution.py:280
  688.7 251.4 %reduce-scatter.10.cloned.1.call-start = ((), (), s32[]{:S(2)}) async-start(), calls=%async_computation.16 | async-start | bytes 11059200 | tf_op jit(solution)/shard_map/reduce_scatter | solution.py:280
  689.4 292.7 %reduce-scatter.8.cloned.1.call-start = ((), (), s32[]{:S(2)}) async-start(), calls=%async_computation.15 | async-start | bytes 3686400 | tf_op jit(solution)/shard_map/reduce_scatter | solution.py:280
  690.2 396.3 %reduce-scatter.14.cloned.1.call-start = ((), (), s32[]{:S(2)}) async-start(), calls=%async_computation.18 | async-start | bytes 11059200 | tf_op jit(solution)/shard_map/reduce_scatter | solution.py:280
  709.2 31.7 %collective-permute-start.22 = (bf16[2,512,640]{2,1,0:T(8,128)(2,1)S(1)}, bf16[2,512,640]{2,1,0:T(8,128)(2,1)S(1)}, u32[]{:S(2)}, u32[]{:S(2)}) collective-permute-start(bf16[2,512,640]{2,1,0:T(8,128)(2,1)S(1)} %pad_maximum_fusion.5), channel_id=1, source_target_pairs={{0,1},{1,0},{2,3},{3,2},{4,5},{5,4},{6,7},{7,6},{8,9},{9,8},{10,11... | collective-permute-start | bytes 3932168 | tf_op jit(solution)/shard_map/ppermute | solution.py:37
  714.9 47.7 %copy-start.31 = (bf16[1024,2560]{1,0:T(8,128)(2,1)}, bf16[1024,2560]{1,0:T(8,128)(2,1)S(1)}, u32[]{:S(2)}) copy-start(bf16[1024,2560]{1,0:T(8,128)(2,1)S(1)} %convolution_convert_fusion.5) | copy-start | bytes 15728644
  715.3 47.3 %collective-permute-start.34 = (bf16[2,512,640]{2,1,0:T(8,128)(2,1)S(1)}, bf16[2,512,640]{2,1,0:T(8,128)(2,1)S(1)}, u32[]{:S(2)}, u32[]{:S(2)}) collective-permute-start(bf16[2,512,640]{2,1,0:T(8,128)(2,1)S(1)} %pad_maximum_fusion.7), channel_id=1, source_target_pairs={{0,1},{1,0},{2,3},{3,2},{4,5},{5,4},{6,7},{7,6},{8,9},{9,8},{10,11... | collective-permute-start | bytes 3932168 | tf_op jit(solution)/shard_map/ppermute | solution.py:37
  717.7 47.4 %copy-start.44 = (bf16[320]{0:T(512)(128)(2,1)S(1)}, bf16[320]{0:T(512)(128)(2,1)}, u32[]{:S(2)}) copy-start(bf16[320]{0:T(512)(128)(2,1)} %param.12) | copy-start | bytes 1924
  717.7 47.4 %copy-start.45 = (bf16[320]{0:T(512)(128)(2,1)S(1)}, bf16[320]{0:T(512)(128)(2,1)}, u32[]{:S(2)}) copy-start(bf16[320]{0:T(512)(128)(2,1)} %param.15) | copy-start | bytes 1924
  717.7 47.4 %collective-permute-start.24 = (bf16[2,512,640]{2,1,0:T(8,128)(2,1)}, bf16[2,512,640]{2,1,0:T(8,128)(2,1)}, u32[]{:S(2)}, u32[]{:S(2)}) collective-permute-start(bf16[2,512,640]{2,1,0:T(8,128)(2,1)} %pad_maximum_fusion.6), channel_id=1, source_target_pairs={{0,2},{1,3},{2,0},{3,1},{4,6},{5,7},{6,4},{7,5},{8,10},{9,11},{10,... | collective-permute-start | bytes 3932168 | tf_op jit(solution)/shard_map/ppermute | solution.py:37
  719.8 78.2 %collective-permute-start.36 = (bf16[2,512,640]{2,1,0:T(8,128)(2,1)}, bf16[2,512,640]{2,1,0:T(8,128)(2,1)}, u32[]{:S(2)}, u32[]{:S(2)}) collective-permute-start(bf16[2,512,640]{2,1,0:T(8,128)(2,1)} %pad_maximum_fusion.8), channel_id=1, source_target_pairs={{0,2},{1,3},{2,0},{3,1},{4,6},{5,7},{6,4},{7,5},{8,10},{9,11},{10,... | collective-permute-start | bytes 3932168 | tf_op jit(solution)/shard_map/ppermute | solution.py:37
  743.5 52.8 %copy-start.26 = (bf16[4,256,768]{2,1,0:T(8,128)(2,1)S(1)}, bf16[4,256,768]{2,1,0:T(8,128)(2,1)}, u32[]{:S(2)}) copy-start(bf16[4,256,768]{2,1,0:T(8,128)(2,1)} %copy-done.25) | copy-start | bytes 4718596
  743.5 48.3 %collective-permute-start.23 = (bf16[512,640]{1,0:T(8,128)(2,1)}, bf16[512,640]{1,0:T(8,128)(2,1)}, u32[]{:S(2)}, u32[]{:S(2)}) collective-permute-start(bf16[512,640]{1,0:T(8,128)(2,1)} %fusion.21), channel_id=1, source_target_pairs={{0,2},{1,3},{2,0},{3,1},{4,6},{5,7},{6,4},{7,5},{8,10},{9,11},{10,... | collective-permute-start | bytes 1966088 | tf_op jit(solution)/shard_map/ppermute | solution.py:37
  763.8 35.4 %collective-permute-start.35 = (bf16[512,640]{1,0:T(8,128)(2,1)}, bf16[512,640]{1,0:T(8,128)(2,1)}, u32[]{:S(2)}, u32[]{:S(2)}) collective-permute-start(bf16[512,640]{1,0:T(8,128)(2,1)} %fusion.17), channel_id=1, source_target_pairs={{0,2},{1,3},{2,0},{3,1},{4,6},{5,7},{6,4},{7,5},{8,10},{9,11},{10,... | collective-permute-start | bytes 1966088 | tf_op jit(solution)/shard_map/ppermute | solution.py:37
  795.4 18.8 %collective-permute-start.25 = (bf16[512,640]{1,0:T(8,128)(2,1)}, bf16[512,640]{1,0:T(8,128)(2,1)}, u32[]{:S(2)}, u32[]{:S(2)}) collective-permute-start(bf16[512,640]{1,0:T(8,128)(2,1)} %get-tuple-element.58), channel_id=1, source_target_pairs={{0,1},{1,0},{2,3},{3,2},{4,5},{5,4},{6,7},{7,6},{8,9},{9,8},{10,11... | collective-permute-start | bytes 1966088 | tf_op jit(solution)/shard_map/ppermute | solution.py:37
  796.8 16.0 %collective-permute-start.38 = (f32[4,256]{1,0:T(4,128)S(1)}, f32[4,256]{1,0:T(4,128)S(1)}, u32[]{:S(2)}, u32[]{:S(2)}) collective-permute-start(f32[4,256]{1,0:T(4,128)S(1)} %dynamic_update_slice.85), channel_id=1, source_target_pairs={{0,1},{1,0},{2,3},{3,2},{4,5},{5,4},{6,7},{7,6},{8,9},{9,8},{10,11... | collective-permute-start | bytes 12296 | tf_op jit(solution)/shard_map/ppermute | solution.py:37
  802.6 17.1 %collective-permute-start.37 = (bf16[512,640]{1,0:T(8,128)(2,1)S(1)}, bf16[512,640]{1,0:T(8,128)(2,1)S(1)}, u32[]{:S(2)}, u32[]{:S(2)}) collective-permute-start(bf16[512,640]{1,0:T(8,128)(2,1)S(1)} %get-tuple-element.52), channel_id=1, source_target_pairs={{0,1},{1,0},{2,3},{3,2},{4,5},{5,4},{6,7},{7,6},{8,9},{9,8},{10,11... | collective-permute-start | bytes 1966088 | tf_op jit(solution)/shard_map/ppermute | solution.py:37
  813.1 3.9 collective-permute-start.39
  824.5 122.4 %copy-start.17 = (bf16[1024,640]{1,0:T(8,128)(2,1)S(1)}, bf16[1024,640]{1,0:T(8,128)(2,1)}, u32[]{:S(2)}) copy-start(bf16[1024,640]{1,0:T(8,128)(2,1)} %param.10) | copy-start | bytes 3932164
  824.5 122.4 %copy-start.20 = (f32[512,640]{1,0:T(8,128)S(1)}, f32[512,640]{1,0:T(8,128)}, u32[]{:S(2)}) copy-start(f32[512,640]{1,0:T(8,128)} %copy-done.18) | copy-start | bytes 3932164
  824.5 126.9 %collective-permute-start.40 = (f32[320]{0:T(512)S(1)}, f32[320]{0:T(512)S(1)}, u32[]{:S(2)}, u32[]{:S(2)}) collective-permute-start(f32[320]{0:T(512)S(1)} %get-tuple-element.92), channel_id=1, source_target_pairs={{0,1},{1,0},{2,3},{3,2},{4,5},{5,4},{6,7},{7,6},{8,9},{9,8},{10,11... | collective-permute-start | bytes 3848 | tf_op jit(solution)/shard_map/ppermute | solution.py:37
  945.4 7.6 collective-permute-start.42
  951.5 32.6 %collective-permute-start.41 = (f32[320]{0:T(512)S(1)}, f32[320]{0:T(512)S(1)}, u32[]{:S(2)}, u32[]{:S(2)}) collective-permute-start(f32[320]{0:T(512)S(1)} %add.362), channel_id=1, source_target_pairs={{0,2},{1,3},{2,0},{3,1},{4,6},{5,7},{6,4},{7,5},{8,10},{9,11},{10,... | collective-permute-start | bytes 3848 | tf_op jit(solution)/shard_map/ppermute | solution.py:37
  953.1 136.2 %collective-permute-start.43 = (f32[320]{0:T(512)S(1)}, f32[320]{0:T(512)S(1)}, u32[]{:S(2)}, u32[]{:S(2)}) collective-permute-start(f32[320]{0:T(512)S(1)} %add.365), channel_id=1, source_target_pairs={{0,2},{1,3},{2,0},{3,1},{4,6},{5,7},{6,4},{7,5},{8,10},{9,11},{10,... | collective-permute-start | bytes 3848 | tf_op jit(solution)/shard_map/ppermute | solution.py:37
  (44 other events, 427.0 us)
Sparse Core Ops, SparseCore 0:
  10.2 47.4 all-gather.5
  59.3 38.1 all-gather.7
  99.7 92.8 all-gather.9
  194.6 92.3 all-gather.11
  288.5 92.3 all-gather.13
  688.0 44.2 reduce-scatter.5
  734.7 101.3 reduce-scatter.11
  838.4 101.5 reduce-scatter.9
  942.4 39.7 reduce-scatter.7
  984.3 102.0 reduce-scatter.13

commit v2 on v1

--- a/solution.py
+++ b/solution.py
@@ -241,6 +241,90 @@
     )(first, qkv, kv, cos, sin, pos, att, d_att, norm)
 
 
+def pair_kernel(core_ref, rows_ref, right_ref, kept_ref, sent_ref):
+    total = tn(rows_ref[...], right_ref[...]).astype(BF16)
+    half = total.shape[0] // 2
+
+    @pl.when(core_ref[0] == 0)
+    def _():
+        kept_ref[...] = total[:half]
+        sent_ref[...] = total[half:]
+
+    @pl.when(core_ref[0] == 1)
+    def _():
+        kept_ref[...] = total[half:]
+        sent_ref[...] = total[:half]
+
+
+def pair_grad(left, right):
+    tokens, rows = left.shape
+    cols = right.shape[1]
+    pairs = lax.axis_size("tok") // 2
+    core = lax.axis_index("tok") % 2
+    step = rows // pairs
+    if step % 128:
+        total = tn(left, right).astype(BF16).reshape(pairs, 2, step // 2, cols)
+        kept, sent = (
+            lax.dynamic_index_in_dim(total, index, 1, False).reshape(-1, cols)
+            for index in (core, 1 - core)
+        )
+        return kept, sent
+    out = jax.ShapeDtypeStruct((rows // 2, cols), BF16)
+    out_spec = pl.BlockSpec((step // 2, cols), lambda pair: (pair, 0))
+    return pl.pallas_call(
+        pair_kernel,
+        grid=(pairs,),
+        out_shape=(out, out),
+        in_specs=[
+            pl.BlockSpec(memory_space=pltpu.SMEM),
+            pl.BlockSpec((tokens, step), lambda pair: (0, pair)),
+            pl.BlockSpec((tokens, cols), lambda pair: (0, 0)),
+        ],
+        out_specs=(out_spec, out_spec),
+        compiler_params=pltpu.CompilerParams(
+            dimension_semantics=("arbitrary",), vmem_limit_bytes=48 << 20
+        ),
+        cost_estimate=pl.CostEstimate(
+            flops=2 * tokens * rows * cols,
+            bytes_accessed=2 * (tokens * rows + tokens * cols + rows * cols),
+            transcendentals=0,
+        ),
+        name="pair_grad",
+    )(core.astype(jnp.int32).reshape(1), left, right)
+
+
+def two_kernel(gate_ref, up_ref, weight_ref, out_ref):
+    cols = gate_ref.shape[1]
+    out_ref[...] = (
+        nt(gate_ref[...], weight_ref[:, :cols]) + nt(up_ref[...], weight_ref[:, cols:])
+    ).astype(BF16)
+
+
+def two_products(d_gate, d_up, weight):
+    tokens, cols = d_gate.shape
+    rows = weight.shape[0]
+    if cols % 128:
+        return (nt(d_gate, weight[:, :cols]) + nt(d_up, weight[:, cols:])).astype(BF16)
+    step = 512
+    whole = pl.BlockSpec((tokens, cols), lambda row: (0, 0))
+    return pl.pallas_call(
+        two_kernel,
+        grid=(rows // step,),
+        out_shape=jax.ShapeDtypeStruct((tokens, rows), BF16),
+        in_specs=[whole, whole, pl.BlockSpec((step, 2 * cols), lambda row: (row, 0))],
+        out_specs=pl.BlockSpec((tokens, step), lambda row: (0, row)),
+        compiler_params=pltpu.CompilerParams(
+            dimension_semantics=("arbitrary",), vmem_limit_bytes=48 << 20
+        ),
+        cost_estimate=pl.CostEstimate(
+            flops=4 * tokens * rows * cols,
+            bytes_accessed=4 * tokens * cols + 4 * rows * cols + 2 * tokens * rows,
+            transcendentals=0,
+        ),
+        name="two_products",
+    )(d_gate, d_up, weight)
+
+
 def after(value, *earlier):
     return lax.optimization_barrier((value, *earlier))[0]
 
@@ -280,10 +364,22 @@
         total = lax.psum_scatter(grad, "tok", scatter_dimension=dim, tiled=True)
         return total.astype(F32)
 
-    w_qkv = from_tok(scaled(qkv_weight, norm1_gain), 0)
-    w_out = from_tok(out_weight, 1)
-    w_gate = from_tok(scaled(gate_weight, norm2_gain), 0)
-    w_up = from_tok(scaled(up_weight, norm2_gain), 0)
+    def pair_to_tok(local):
+        kept, sent = local
+        count = lax.axis_size("tok")
+        got = lax.ppermute(sent, "tok", [(i, i ^ 1) for i in range(count)])
+        both = (kept.astype(F32) + got.astype(F32)).astype(BF16)
+        groups = [list(range(core, count, 2)) for core in range(2)]
+        total = lax.psum_scatter(
+            both, "tok", scatter_dimension=0, tiled=True, axis_index_groups=groups
+        )
+        return total.astype(F32)
+
+    qkv_cols, ff_cols = qkv_weight.shape[1], gate_weight.shape[1]
+    w_attn = from_tok(jnp.concatenate([scaled(qkv_weight, norm1_gain), out_weight.T], axis=1), 0)
+    w_qkv, w_out_t = w_attn[:, :qkv_cols], w_attn[:, qkv_cols:]
+    gu_local = jnp.concatenate([scaled(w, norm2_gain) for w in (gate_weight, up_weight)], 1)
+    w_gu = from_tok(gu_local, 0)
     w_down = from_tok(down_weight, 1)
 
     rows_in = gather_mdl(inputs, 1)
@@ -302,43 +398,42 @@
     attended, log_norm = attention_forward(first, qkv, kv, cos, sin, pos)
     head_block = cols_to_rows(attended)
     residual = inputs.astype(F32)
-    mixed = residual + scatter_mdl(nn(head_block, w_out).astype(BF16), 1)
+    mixed = residual + scatter_mdl(nt(head_block, w_out_t).astype(BF16), 1)
 
     rows_two = gather_mdl(mixed.astype(BF16), 1)
     scale_two = row_scale(rows_two)
-    gate_in = nn(rows_two, w_gate) * scale_two
-    up_in = nn(rows_two, w_up) * scale_two
+    rows_hat = (rows_two.astype(F32) * scale_two).astype(BF16)
+    gate_in = nn(rows_hat, w_gu[:, :ff_cols])
+    up_in = nn(rows_hat, w_gu[:, ff_cols:])
     gelu, _ = gelu_parts(gate_in)
     hidden = (gelu * up_in).astype(BF16)
     gate_in, up_in, hidden = lax.optimization_barrier((gate_in, up_in, hidden))
     gelu, slope = gelu_parts(gate_in)
 
-    down_local = tn(hidden, cotangent).astype(BF16)
-    down_grad = to_tok(down_local, 1)
+    down_local = pair_grad(cotangent, hidden)
+    down_grad = pair_to_tok(down_local).T
     d_hidden = nt(cotangent, w_down)
-    d_gate = d_hidden * up_in * slope
-    d_up = d_hidden * gelu
-    stat_two = jnp.sum(d_gate * gate_in + d_up * up_in, axis=1)
-    gate_scaled = (d_gate * scale_two).astype(BF16)
-    up_scaled = (d_up * scale_two).astype(BF16)
-    d_two_part = (nt(d_gate.astype(BF16), w_gate) + nt(d_up.astype(BF16), w_up)).astype(BF16)
-    rows_later = after(rows_two, d_two_part)
-    gate_local = tn(rows_later, gate_scaled).astype(BF16)
-    gate_sum = to_tok(gate_local, 0)
-    rows_later = after(rows_two, gate_local)
-    up_local = tn(rows_later, up_scaled).astype(BF16)
-    up_sum = to_tok(up_local, 0)
+    d_gate_f = d_hidden * up_in * slope
+    d_up_f = d_hidden * gelu
+    stat_two = jnp.sum(d_gate_f * gate_in + d_up_f * up_in, axis=1)
+    d_gate, d_up = d_gate_f.astype(BF16), d_up_f.astype(BF16)
+    gate_local = pair_grad(rows_hat, d_gate)
+    gate_sum = pair_to_tok(gate_local)
+    d_two_part = two_products(d_gate, d_up, w_gu)
+    rows_later = after(rows_hat, d_two_part)
+    up_local = pair_grad(rows_later, d_up)
+    up_sum = pair_to_tok(up_local)
     d_two = scatter_mdl(d_two_part, 1)
     stat_two = sum_mdl(stat_two.reshape(8, -1)).reshape(-1, 1) * (1.0 / features)
     scale_mixed = scale_two * mixed
     cotangent_own = lax.dynamic_slice_in_dim(cotangent, me * width, width, 1).astype(F32)
     d_mixed = cotangent_own + scale_two * (d_two - scale_mixed * stat_two)
 
-    d_mixed_b = after(d_mixed.astype(BF16), up_local)
+    d_mixed_b = after(d_mixed.astype(BF16), up_local[0])
     d_mixed_rows = gather_mdl(d_mixed_b, 1)
     hidden_later = after(hidden, d_mixed_b)
     ffn_part = nn(hidden_later, w_down).astype(BF16)
-    d_head = nt(after(d_mixed_rows, ffn_part), w_out).astype(BF16)
+    d_head = nn(after(d_mixed_rows, ffn_part), w_out_t).astype(BF16)
     d_attended = rows_to_cols(d_head)
     out_local = tn(d_mixed_rows, after(head_block, d_head)).astype(BF16)
     out_grad = to_tok(out_local, 0).T
@@ -361,7 +456,7 @@
     input_grad = d_mixed + scale_one * (d_one - (scale_one * residual) * stat_one)
 
     norm1_late, norm2_late, qkv_late, gate_late, up_late, _ = lax.optimization_barrier(
-        (norm1_gain, norm2_gain, qkv_weight, gate_weight, up_weight, up_local)
+        (norm1_gain, norm2_gain, qkv_weight, gate_weight, up_weight, up_local[0])
     )
 
     def unfold(total, gain):

time: 1110 us -> 865 us (0.78)
  waiting for transfers between devices: 652 us -> 401 us
  matrix products: 231 us -> 125 us
  Pallas kernels: 26.5 us -> 102 us
  other arithmetic: 62.7 us -> 77.5 us
  blocking collectives: 18.8 us -> 32.9 us
    reduce_scatter x5 -> x2, waiting for transfers between devices: 245 us -> 0.01 us  [to_tok(): total = lax.psum_scatter(grad, 'tok', scatter_dimension=dim, tiled=True)]
    pallas_call x0 -> x4, Pallas kernels: none -> 75.8 us  [the longest x3 47.8 us: pair_grad(): pl.pallas_call(pair_kernel, grid=(pairs,), out_shape=(out, out), in_specs...]
    dot_general x5 -> x2, matrix products: 81.7 us -> 17.6 us  [tn(): lax.dot_general(left_op, right_op, (((0,), (0,)), ((), ())), preferred_el...]
    dot_general x5 -> x3, matrix products: 79.7 us -> 36.5 us  [nt(): lax.dot_general(left_op, right_op, (((1,), (1,)), ((), ())), preferred_el...]
    all_gather x5 -> x3, waiting for transfers between devices: 78.2 us -> 45.7 us  [from_tok(): return lax.all_gather(weight, 'tok', axis=dim, tiled=True)]
    convert_element_type x2 -> x5, other arithmetic: 7.42 us -> 27.7 us  [the longest x3 17.8 us: pair_to_tok(): both = (kept.astype(F32) + got.astype(F32)).astype(BF16)]
    ppermute x44, waiting for transfers between devices: 290 us -> 309 us  [swap(): return lax.ppermute(block, 'mdl', [(i, i ^ distance) for i in range(size)])]
    ppermute x0 -> x3, waiting for transfers between devices: none -> 17 us  [pair_to_tok(): got = lax.ppermute(sent, 'tok', [(i, i ^ 1) for i in range(count)])]
  transfers between devices with their start and end apart: 57 -> 57, of which waited for: 32 -> 36; matrix products, arithmetic and copies ran while one was open for 19% -> 23% of each run, Pallas kernels for 1% -> 10%
where the time goes in v2:
time: 865 us; the launch traced here: 856 us
  waiting for transfers between devices  401 us (46%)
  matrix products  125 us (14%)
  Pallas kernels  102 us (12%)
  other arithmetic  77.5 us (9%)
  starting transfers between devices  62 us (7%)
  local copies, waits for them, and re-layouts  38.9 us (4%)
  blocking collectives  32.9 us (4%)
  between operations  15.6 us (2%)
    ppermute x44, waiting for transfers between devices, swap(): return lax.ppermute(block, 'mdl', [(i, i ^ distance) for i in range(size)])  309 us
    dot_general x5, matrix products, nn(): return jnp.dot(left_op, right_op, preferred_element_type=F32)  71.4 us
    ppermute x44, starting transfers between devices, swap(): return lax.ppermute(block, 'mdl', [(i, i ^ distance) for i in range(size)])  53 us
    pallas_call x3, Pallas kernels, pair_grad(): pl.pallas_call(pair_kernel, grid=(pairs,), out_shape=(out, out), in_specs...  47.8 us
    all_gather x3, waiting for transfers between devices, from_tok(): return lax.all_gather(weight, 'tok', axis=dim, tiled=True)  45.7 us
    dot_general x3, matrix products, nt(): lax.dot_general(left_op, right_op, (((1,), (1,)), ((), ())), preferred_el...  36.5 us
    all_to_all x2, blocking collectives, cols_to_rows(): return lax.all_to_all(block, 'mdl', split_axis=1, concat_axis=0, tiled=True)  32.9 us
    pallas_call x1, Pallas kernels, two_products(): pl.pallas_call(two_kernel, grid=(rows // step,), out_shape=jax.ShapeDtype...  28 us
  transfers between devices with their start and end apart: 57, of which 36 were waited for; matrix products, arithmetic and copies ran while one was open for 23% of the time, Pallas kernels for 10%

profile of v2, /device:TPU:0, one launch (start us, length us, event | category | flops | bytes accessed | tf_op | source)
XLA Modules:
  0.0 856.4 jit_solution(8792164758291490853)
XLA Ops:
  13.8 3.0 collective-permute-start
  18.3 27.3 %collective-permute-done = bf16[1024,640]{1,0:T(8,128)(2,1)S(1)} collective-permute-done((bf16[1024,640]{1,0:T(8,128)(2,1)S(1)}, bf16[1024,640]{1,0:T(8,128)(2,1)S(1)}, u32[]{:S(2)}, u32[]{:S(2)}) %collective-permute-start) | collective-permute-done | bytes 1310752 | tf_op jit(solution)/shard_map/ppermute | solution.py:37
  53.6 9.1 %collective-permute-done.2 = bf16[512,640]{1,0:T(8,128)(2,1)S(1)} collective-permute-done((bf16[512,640]{1,0:T(8,128)(2,1)}, bf16[512,640]{1,0:T(8,128)(2,1)S(1)}, u32[]{:S(2)}, u32[]{:S(2)}) %collective-permute-start.2) | collective-permute-done | bytes 655392 | tf_op jit(solution)/shard_map/ppermute | solution.py:37
  62.7 3.2 collective-permute-done.3
  69.4 17.0 %all-gather.4.cloned.1.call-done = bf16[2560,1408]{1,0:T(8,128)(2,1)} async-done(((bf16[320,1408]{1,0:T(8,128)(2,1)}), bf16[2560,1408]{1,0:T(8,128)(2,1)}) %all-gather.4.cloned.1.call-update) | async-done | bytes 7208976 | tf_op jit(solution)/shard_map/all_gather | solution.py:361
  86.4 9.0 %multiply_convert_fusion.2 = bf16[1024,768]{1,0:T(8,128)(2,1)} fusion(bf16[1024,2560]{1,0:T(8,128)(2,1)} %copy-done.27, bf16[2560,1408]{1,0:T(8,128)(2,1)} %all-gather.4.cloned.1.call-done, f32[1024]{0:T(1024)S(1)} %add_rsqrt_fusion.1), kind=kOutput, calls=%fused_computation.32 | convolution fusion | flops 4028104704 | bytes 10752000 | tf_op jit(solution)/shard_map/dot_general | solution.py:32
  95.5 3.8 all-to-all-start
  100.1 19.0 %all-to-all-done = bf16[4,256,768]{2,1,0:T(8,128)(2,1)S(1)} async-done(((bf16[4,256,768]{2,1,0:T(8,128)(2,1)}), bf16[4,256,768]{2,1,0:T(8,128)(2,1)S(1)}, u32[]{:S(2)}, u32[]{:S(2)}) %all-to-all-start) | async-done | bytes 1572896 | tf_op jit(solution)/shard_map/all_to_all | solution.py:111
  123.9 5.7 collective-permute-done.4
  131.8 2.8 collective-permute-done.6
  136.2 10.8 %attention_forward.1 = (bf16[256,2560]{1,0:T(8,128)(2,1)S(1)}, f32[10,256,1]{2,1,0:T(8,128)S(1)}) custom-call(s32[1]{0:T(128)} %bitcast.first_ref, bf16[256,3072]{1,0:T(8,128)(2,1)S(1)} %bitcast.197, bf16[1024,512]{1,0:T(8,128)(2,1)S(1)} %constant_dynamic-update-slice_fusion.8.kv_ref, f32[256,128]{1,0:T(8,128)S(1)} %get-tuple-element.115.cos_ref, ...), custom_call_target="tpu_custom_call" | custom-call | flops 2684354560 | bytes 3670016 | tf_op jit(solution)/shard_map/attention_forward/pallas_call | solution.py:182
  147.2 17.6 %all_to_all.76 = bf16[256,4,640]{2,0,1:T(8,128)(2,1)S(1)} all-to-all(bf16[256,4,640]{2,0,1:T(8,128)(2,1)S(1)} %bitcast.205), channel_id=1, replica_groups=mesh['tok'=8,'mdl'=4] {'mdl'}, dimensions={1} | all-to-all | bytes 2621440 | tf_op jit(solution)/shard_map/all_to_all | solution.py:115
  164.8 7.1 convolution_convert_fusion.1
  174.1 25.5 %collective-permute-done.8 = bf16[2,512,640]{2,1,0:T(8,128)(2,1)S(1)} collective-permute-done((bf16[2,512,640]{2,1,0:T(8,128)(2,1)S(1)}, bf16[2,512,640]{2,1,0:T(8,128)(2,1)S(1)}, u32[]{:S(2)}, u32[]{:S(2)}) %collective-permute-start.8) | collective-permute-done | bytes 1310752 | tf_op jit(solution)/shard_map/ppermute | solution.py:37
  203.3 11.4 %collective-permute-done.9 = bf16[512,640]{1,0:T(8,128)(2,1)S(1)} collective-permute-done((bf16[512,640]{1,0:T(8,128)(2,1)S(1)}, bf16[512,640]{1,0:T(8,128)(2,1)S(1)}, u32[]{:S(2)}, u32[]{:S(2)}) %collective-permute-start.9) | collective-permute-done | bytes 655392 | tf_op jit(solution)/shard_map/ppermute | solution.py:37
  216.0 13.5 %collective-permute-done.11 = bf16[512,640]{1,0:T(8,128)(2,1)S(1)} collective-permute-done((bf16[512,640]{1,0:T(8,128)(2,1)S(1)}, bf16[512,640]{1,0:T(8,128)(2,1)S(1)}, u32[]{:S(2)}, u32[]{:S(2)}) %collective-permute-start.11) | collective-permute-done | bytes 655392 | tf_op jit(solution)/shard_map/ppermute | solution.py:37
  229.8 2.6 broadcast.71.clone
  236.3 25.4 %collective-permute-done.12 = bf16[1024,640]{1,0:T(8,128)(2,1)S(1)} collective-permute-done((bf16[1024,640]{1,0:T(8,128)(2,1)S(1)}, bf16[1024,640]{1,0:T(8,128)(2,1)S(1)}, u32[]{:S(2)}, u32[]{:S(2)}) %collective-permute-start.12) | collective-permute-done | bytes 1310752 | tf_op jit(solution)/shard_map/ppermute | solution.py:37
  267.9 2.8 constant_dynamic-update-slice_fusion.6
  271.9 4.6 collective-permute-done.14
  281.1 3.6 fusion
  284.7 5.8 fusion.1.rows_ref
  290.6 17.3 %fusion.4 = f32[1024,1920]{1,0:T(8,128)} fusion(bf16[1024,2560]{1,0:T(8,128)(2,1)} %fusion.1.rows_ref, bf16[2560,3840]{1,0:T(8,128)(2,1)} %all-gather.6.cloned.1.call-done.weight_ref), kind=kOutput, calls=%fused_computation.7 | convolution fusion | flops 10066329600 | bytes 22937600 | tf_op jit(solution)/shard_map/dot_general | solution.py:32
  307.8 19.3 %multiply_convert_fusion = (bf16[1024,1920]{1,0:T(8,128)(2,1)}, f32[1024,1920]{1,0:T(8,128)}) fusion(f32[1024,1920]{1,0:T(8,128)} %fusion.4, bf16[1024,2560]{1,0:T(8,128)(2,1)S(1)} %copy-done.31, bf16[2560,3840]{1,0:T(8,128)(2,1)} %all-gather.6.cloned.1.call-done.weight_ref), kind=kOutput, calls=%fused_computation.18 | convolution fusion | flops 10085990400 | bytes 34734080 | tf_op jit(solution)/shard_map/dot_general | solution.py:32
  327.2 28.6 %all-gather.8.cloned.1.call-done = bf16[1920,2560]{0,1:T(8,128)(2,1)} async-done(((bf16[1920,320]{0,1:T(8,128)(2,1)}), bf16[1920,2560]{0,1:T(8,128)(2,1)}) %all-gather.8.cloned.1.call-update) | async-done | bytes 9830416 | tf_op jit(solution)/shard_map/all_gather | solution.py:361
  355.8 22.8 %fusion.70 = (bf16[1024,1920]{1,0:T(8,128)(2,1)S(1)}, f32[1024]{0:T(1024)S(1)}, bf16[1024,1920]{1,0:T(8,128)(2,1)}) fusion(f32[1024,1920]{1,0:T(8,128)} %fusion.4, f32[1024,1920]{1,0:T(8,128)} %get-tuple-element.35, bf16[1024,2560]{1,0:T(8,128)(2,1)} %rows_ref.1, bf16[1920,2560]{0,1:T(8,128)(2,1)} %all-gather.8.cloned.1.call-done), kind=kOutput, calls=%fused_computation.213 | convolution fusion | flops 10117446656 | bytes 38670336 | tf_op jit(solution)/shard_map/dot_general | solution.py:20
  378.6 16.8 %pair_grad.4 = (bf16[1280,1920]{1,0:T(8,128)(2,1)}, bf16[1280,1920]{1,0:T(8,128)(2,1)}) custom-call(s32[1]{0:T(128)} %bitcast.25.core_ref, bf16[1024,2560]{1,0:T(8,128)(2,1)} %fusion.1.rows_ref, bf16[1024,1920]{1,0:T(8,128)(2,1)S(1)} %get-tuple-element.61.gate_ref.right_ref), custom_call_target="tpu_custom_call" | custom-call | flops 10066329600 | bytes 19005440 | tf_op jit(solution)/shard_map/pair_grad/pallas_call | solution.py:274
  395.7 8.2 collective-permute-done.42
  403.8 5.9 add_convert_fusion.2
  412.0 28.0 %two_products.1 = bf16[1024,2560]{1,0:T(8,128)(2,1)} custom-call(bf16[1024,1920]{1,0:T(8,128)(2,1)S(1)} %copy-done.17, bf16[1024,1920]{1,0:T(8,128)(2,1)} %get-tuple-element.63.up_ref.right_ref, bf16[2560,3840]{1,0:T(8,128)(2,1)} %all-gather.6.cloned.1.call-done.weight_ref), custom_call_target="tpu_custom_call" | custom-call | flops 20132659200 | bytes 32768000 | tf_op jit(solution)/shard_map/two_products/pallas_call | solution.py:310
  440.0 15.6 %pair_grad.3 = (bf16[1280,1920]{1,0:T(8,128)(2,1)}, bf16[1280,1920]{1,0:T(8,128)(2,1)}) custom-call(s32[1]{0:T(128)} %bitcast.25.core_ref, bf16[1024,2560]{1,0:T(8,128)(2,1)} %fusion.1.rows_ref, bf16[1024,1920]{1,0:T(8,128)(2,1)S(1)} %copy-done.15), custom_call_target="tpu_custom_call" | custom-call | flops 10066329600 | bytes 19005440 | tf_op jit(solution)/shard_map/pair_grad/pallas_call | solution.py:274
  459.3 27.9 %collective-permute-done.16 = bf16[2,512,640]{2,1,0:T(8,128)(2,1)S(1)} collective-permute-done((bf16[2,512,640]{2,1,0:T(8,128)(2,1)S(1)}, bf16[2,512,640]{2,1,0:T(8,128)(2,1)S(1)}, u32[]{:S(2)}, u32[]{:S(2)}) %collective-permute-start.16) | collective-permute-done | bytes 1310752 | tf_op jit(solution)/shard_map/ppermute | solution.py:37
  488.7 14.8 %collective-permute-done.17 = bf16[512,640]{1,0:T(8,128)(2,1)S(1)} collective-permute-done((bf16[512,640]{1,0:T(8,128)(2,1)S(1)}, bf16[512,640]{1,0:T(8,128)(2,1)S(1)}, u32[]{:S(2)}, u32[]{:S(2)}) %collective-permute-start.17) | collective-permute-done | bytes 655392 | tf_op jit(solution)/shard_map/ppermute | solution.py:37
  506.1 13.4 %collective-permute-done.20 = f32[8,128]{1,0:T(8,128)S(1)} collective-permute-done((f32[8,128]{1,0:T(8,128)S(1)}, f32[8,128]{1,0:T(8,128)S(1)}, u32[]{:S(2)}, u32[]{:S(2)}) %collective-permute-start.20) | collective-permute-done | bytes 4128 | tf_op jit(solution)/shard_map/ppermute | solution.py:37
  523.4 4.1 fusion.71
  530.3 6.0 add_convert_fusion.1
  536.3 18.8 %collective-permute-done.26 = bf16[1024,640]{1,0:T(8,128)(2,1)S(1)} collective-permute-done((bf16[1024,640]{1,0:T(8,128)(2,1)}, bf16[1024,640]{1,0:T(8,128)(2,1)S(1)}, u32[]{:S(2)}, u32[]{:S(2)}) %collective-permute-start.26) | collective-permute-done | bytes 1310752 | tf_op jit(solution)/shard_map/ppermute | solution.py:37
  560.3 16.7 %convolution_convert_fusion = bf16[1024,2560]{1,0:T(8,128)(2,1)} fusion(bf16[1024,1920]{1,0:T(8,128)(2,1)} %get-tuple-element.40.right_ref, bf16[1920,2560]{0,1:T(8,128)(2,1)} %all-gather.8.cloned.1.call-done), kind=kOutput, calls=%fused_computation.19 | convolution fusion | flops 10068951040 | bytes 19005440 | tf_op jit(solution)/shard_map/dot_general | solution.py:32
  580.9 9.1 %fusion.24 = bf16[1024,640]{1,0:T(8,128)(2,1)} fusion(bf16[1024,2560]{1,0:T(8,128)(2,1)S(1)} %constant_dynamic-update-slice_fusion.17, bf16[2560,1408]{1,0:T(8,128)(2,1)} %all-gather.4.cloned.1.call-done), kind=kOutput, calls=%fused_computation.55 | convolution fusion | flops 3356098560 | bytes 9830400 | tf_op jit(solution)/shard_map/dot_general | solution.py:32
  590.0 4.5 all-to-all-start.2
  594.6 8.5 convolution_convert_fusion.4
  603.1 2.4 all-to-all-done.2
  608.5 15.9 %attention_backward.1 = (bf16[256,2560]{1,0:T(8,128)(2,1)S(1)}, f32[1024,512]{1,0:T(8,128)S(1)}) custom-call(s32[1]{0:T(128)} %bitcast.first_ref, bf16[256,3072]{1,0:T(8,128)(2,1)S(1)} %bitcast.198, bf16[1024,512]{1,0:T(8,128)(2,1)S(1)} %copy-done.5, f32[256,128]{1,0:T(8,128)S(1)} %copy-done.11, f32[256,128]{1,0:T(8,128)S(1)} %copy-done.9, ...), custom_call_target="tpu_custom_call" | custom-call | flops 6710886400 | bytes 8388608 | tf_op jit(solution)/shard_map/attention_backward/pallas_call | solution.py:213
  626.9 5.4 collective-permute-done.30
  633.9 3.5 collective-permute-done.31
  639.0 5.0 collective-permute-done.33
  644.9 15.3 %all_to_all.77 = bf16[256,4,768]{2,0,1:T(8,128)(2,1)S(1)} all-to-all(bf16[256,4,768]{2,0,1:T(8,128)(2,1)S(1)} %bitcast.204), channel_id=1, replica_groups=mesh['tok'=8,'mdl'=4] {'mdl'}, dimensions={1} | all-to-all | bytes 3145728 | tf_op jit(solution)/shard_map/all_to_all | solution.py:115
  660.2 9.0 %convolution_convert_fusion.3 = bf16[2560,768]{1,0:T(8,128)(2,1)} fusion(bf16[1024,2560]{1,0:T(8,128)(2,1)} %copy-done.27, bf16[1024,768]{1,0:T(8,128)(2,1)S(1)} %bitcast.208, f32[1024]{0:T(1024)S(1)} %copy-done.48), kind=kOutput, calls=%fused_computation.22 | convolution fusion | flops 4030857216 | bytes 10752000 | tf_op jit(solution)/shard_map/dot_general | solution.py:26
  672.3 15.4 %pair_grad.5 = (bf16[1280,1920]{1,0:T(8,128)(2,1)}, bf16[1280,1920]{1,0:T(8,128)(2,1)}) custom-call(s32[1]{0:T(128)} %bitcast.25.core_ref, bf16[1024,2560]{1,0:T(8,128)(2,1)} %rows_ref.1, bf16[1024,1920]{1,0:T(8,128)(2,1)S(1)} %copy-done.14), custom_call_target="tpu_custom_call" | custom-call | flops 10066329600 | bytes 19005440 | tf_op jit(solution)/shard_map/pair_grad/pallas_call | solution.py:274
  687.8 8.8 %collective-permute-done.46 = bf16[1280,1920]{1,0:T(8,128)(2,1)S(1)} collective-permute-done((bf16[1280,1920]{1,0:T(8,128)(2,1)}, bf16[1280,1920]{1,0:T(8,128)(2,1)S(1)}, u32[]{:S(2)}, u32[]{:S(2)}) %collective-permute-start.46) | collective-permute-done | bytes 4915232 | tf_op jit(solution)/shard_map/ppermute | solution.py:370
  696.6 5.9 add_convert_fusion
  705.8 6.6 convolution_convert_fusion.2
  717.3 19.1 %collective-permute-done.22 = bf16[2,512,640]{2,1,0:T(8,128)(2,1)S(1)} collective-permute-done((bf16[2,512,640]{2,1,0:T(8,128)(2,1)S(1)}, bf16[2,512,640]{2,1,0:T(8,128)(2,1)S(1)}, u32[]{:S(2)}, u32[]{:S(2)}) %collective-permute-start.22) | collective-permute-done | bytes 1310752 | tf_op jit(solution)/shard_map/ppermute | solution.py:37
  736.4 2.6 fusion.34
  740.0 23.6 %collective-permute-done.34 = bf16[2,512,640]{2,1,0:T(8,128)(2,1)S(1)} collective-permute-done((bf16[2,512,640]{2,1,0:T(8,128)(2,1)S(1)}, bf16[2,512,640]{2,1,0:T(8,128)(2,1)S(1)}, u32[]{:S(2)}, u32[]{:S(2)}) %collective-permute-start.34) | collective-permute-done | bytes 1310752 | tf_op jit(solution)/shard_map/ppermute | solution.py:37
  766.5 21.5 %collective-permute-done.23 = bf16[512,640]{1,0:T(8,128)(2,1)} collective-permute-done((bf16[512,640]{1,0:T(8,128)(2,1)}, bf16[512,640]{1,0:T(8,128)(2,1)}, u32[]{:S(2)}, u32[]{:S(2)}) %collective-permute-start.23) | collective-permute-done | bytes 655392 | tf_op jit(solution)/shard_map/ppermute | solution.py:37
  787.9 3.1 fusion.35
  793.7 6.9 collective-permute-done.35
  800.6 3.1 fusion.31
  809.2 10.1 %collective-permute-done.37 = bf16[512,640]{1,0:T(8,128)(2,1)S(1)} collective-permute-done((bf16[512,640]{1,0:T(8,128)(2,1)}, bf16[512,640]{1,0:T(8,128)(2,1)S(1)}, u32[]{:S(2)}, u32[]{:S(2)}) %collective-permute-start.37) | collective-permute-done | bytes 655392 | tf_op jit(solution)/shard_map/ppermute | solution.py:37
  820.9 3.5 fusion.16
  824.4 5.4 convert_multiply_fusion.3
  838.0 7.1 reduce-scatter.14.cloned.1.call-done
  845.1 2.9 convert_bitcast_fusion
  (304 shorter events, 121.8 us)
Async XLA Ops:
  7.2 79.2 %all-gather.4.cloned.1.call-start = ((), (), s32[]{:S(2)}) async-start(), calls=%async_computation.9 | async-start | bytes 8110080 | tf_op jit(solution)/shard_map/all_gather | solution.py:361
  11.3 279.3 %all-gather.6.cloned.1.call-start = ((), (), s32[]{:S(2)}) async-start(), calls=%async_computation.10 | async-start | bytes 22118400 | tf_op jit(solution)/shard_map/all_gather | solution.py:361
  13.8 31.7 %collective-permute-start = (bf16[1024,640]{1,0:T(8,128)(2,1)S(1)}, bf16[1024,640]{1,0:T(8,128)(2,1)S(1)}, u32[]{:S(2)}, u32[]{:S(2)}) collective-permute-start(bf16[1024,640]{1,0:T(8,128)(2,1)S(1)} %copy-done.18), channel_id=1, source_target_pairs={{0,1},{1,0},{2,3},{3,2},{4,5},{5,4},{6,7},{7,6},{8,9},{9,8},{10,11... | collective-permute-start | bytes 3932168 | tf_op jit(solution)/shard_map/ppermute | solution.py:37
  16.8 31.4 %collective-permute-start.1 = (bf16[1024,640]{1,0:T(8,128)(2,1)S(1)}, bf16[1024,640]{1,0:T(8,128)(2,1)S(1)}, u32[]{:S(2)}, u32[]{:S(2)}) collective-permute-start(bf16[1024,640]{1,0:T(8,128)(2,1)S(1)} %copy-done.18), channel_id=1, source_target_pairs={{0,2},{1,3},{2,0},{3,1},{4,6},{5,7},{6,4},{7,5},{8,10},{9,11},{10,... | collective-permute-start | bytes 3932168 | tf_op jit(solution)/shard_map/ppermute | solution.py:37
  46.4 16.2 %collective-permute-start.2 = (bf16[512,640]{1,0:T(8,128)(2,1)}, bf16[512,640]{1,0:T(8,128)(2,1)S(1)}, u32[]{:S(2)}, u32[]{:S(2)}) collective-permute-start(bf16[512,640]{1,0:T(8,128)(2,1)} %slice.160), channel_id=1, source_target_pairs={{0,2},{1,3},{2,0},{3,1},{4,6},{5,7},{6,4},{7,5},{8,10},{9,11},{10,... | collective-permute-start | bytes 1966088 | tf_op jit(solution)/shard_map/ppermute | solution.py:37
  50.2 15.8 %collective-permute-start.3 = (bf16[512,640]{1,0:T(8,128)(2,1)}, bf16[512,640]{1,0:T(8,128)(2,1)}, u32[]{:S(2)}, u32[]{:S(2)}) collective-permute-start(bf16[512,640]{1,0:T(8,128)(2,1)} %slice.161), channel_id=1, source_target_pairs={{0,1},{1,0},{2,3},{3,2},{4,5},{5,4},{6,7},{7,6},{8,9},{9,8},{10,11... | collective-permute-start | bytes 1966088 | tf_op jit(solution)/shard_map/ppermute | solution.py:37
  69.4 26.1 %copy-start.47 = (f32[1024]{0:T(1024)}, f32[1024]{0:T(1024)S(1)}, u32[]{:S(2)}) copy-start(f32[1024]{0:T(1024)S(1)} %add_rsqrt_fusion.1) | copy-start | bytes 12292
  95.5 23.6 %all-to-all-start = ((bf16[4,256,768]{2,1,0:T(8,128)(2,1)}), bf16[4,256,768]{2,1,0:T(8,128)(2,1)S(1)}, u32[]{:S(2)}, u32[]{:S(2)}) async-start(bf16[4,256,768]{2,1,0:T(8,128)(2,1)} %bitcast.2), calls=%async_computation | async-start | bytes 3145728 | tf_op jit(solution)/shard_map/all_to_all | solution.py:111
  99.3 256.5 %all-gather.8.cloned.1.call-start = ((), (), s32[]{:S(2)}) async-start(), calls=%async_computation.11 | async-start | bytes 11059200 | tf_op jit(solution)/shard_map/all_gather | solution.py:361
  100.0 724.3 %reduce-scatter.10.cloned.1.call-start = ((), (), s32[]{:S(2)}) async-start(), calls=%async_computation.14 | async-start | bytes 6144000 | tf_op jit(solution)/shard_map/reduce_scatter | solution.py:373
  120.9 26.2 %copy-start.8 = (f32[256,128]{1,0:T(8,128)}, f32[256,128]{1,0:T(8,128)S(1)}, u32[]{:S(2)}) copy-start(f32[256,128]{1,0:T(8,128)S(1)} %get-tuple-element.114.sin_ref) | copy-start | bytes 393220
  120.9 26.2 %copy-start.10 = (f32[256,128]{1,0:T(8,128)}, f32[256,128]{1,0:T(8,128)S(1)}, u32[]{:S(2)}) copy-start(f32[256,128]{1,0:T(8,128)S(1)} %get-tuple-element.115.cos_ref) | copy-start | bytes 393220
  121.7 7.8 collective-permute-start.4
  123.1 8.0 collective-permute-start.5
  129.6 5.0 collective-permute-start.6
  131.1 5.0 collective-permute-start.7
  172.3 27.3 %collective-permute-start.8 = (bf16[2,512,640]{2,1,0:T(8,128)(2,1)S(1)}, bf16[2,512,640]{2,1,0:T(8,128)(2,1)S(1)}, u32[]{:S(2)}, u32[]{:S(2)}) collective-permute-start(bf16[2,512,640]{2,1,0:T(8,128)(2,1)S(1)} %pad_maximum_fusion.2), channel_id=1, source_target_pairs={{0,1},{1,0},{2,3},{3,2},{4,5},{5,4},{6,7},{7,6},{8,9},{9,8},{10,11... | collective-permute-start | bytes 3932168 | tf_op jit(solution)/shard_map/ppermute | solution.py:37
  173.4 29.9 %collective-permute-start.10 = (bf16[2,512,640]{2,1,0:T(8,128)(2,1)S(1)}, bf16[2,512,640]{2,1,0:T(8,128)(2,1)S(1)}, u32[]{:S(2)}, u32[]{:S(2)}) collective-permute-start(bf16[2,512,640]{2,1,0:T(8,128)(2,1)S(1)} %pad_maximum_fusion.3), channel_id=1, source_target_pairs={{0,2},{1,3},{2,0},{3,1},{4,6},{5,7},{6,4},{7,5},{8,10},{9,11},{10,... | collective-permute-start | bytes 3932168 | tf_op jit(solution)/shard_map/ppermute | solution.py:37
  199.7 15.1 %collective-permute-start.9 = (bf16[512,640]{1,0:T(8,128)(2,1)S(1)}, bf16[512,640]{1,0:T(8,128)(2,1)S(1)}, u32[]{:S(2)}, u32[]{:S(2)}) collective-permute-start(bf16[512,640]{1,0:T(8,128)(2,1)S(1)} %fusion.42), channel_id=1, source_target_pairs={{0,2},{1,3},{2,0},{3,1},{4,6},{5,7},{6,4},{7,5},{8,10},{9,11},{10,... | collective-permute-start | bytes 1966088 | tf_op jit(solution)/shard_map/ppermute | solution.py:37
  215.2 14.3 %collective-permute-start.11 = (bf16[512,640]{1,0:T(8,128)(2,1)S(1)}, bf16[512,640]{1,0:T(8,128)(2,1)S(1)}, u32[]{:S(2)}, u32[]{:S(2)}) collective-permute-start(bf16[512,640]{1,0:T(8,128)(2,1)S(1)} %get-tuple-element.83), channel_id=1, source_target_pairs={{0,1},{1,0},{2,3},{3,2},{4,5},{5,4},{6,7},{7,6},{8,9},{9,8},{10,11... | collective-permute-start | bytes 1966088 | tf_op jit(solution)/shard_map/ppermute | solution.py:37
  234.1 27.5 %collective-permute-start.12 = (bf16[1024,640]{1,0:T(8,128)(2,1)S(1)}, bf16[1024,640]{1,0:T(8,128)(2,1)S(1)}, u32[]{:S(2)}, u32[]{:S(2)}) collective-permute-start(bf16[1024,640]{1,0:T(8,128)(2,1)S(1)} %get-tuple-element.60), channel_id=1, source_target_pairs={{0,1},{1,0},{2,3},{3,2},{4,5},{5,4},{6,7},{7,6},{8,9},{9,8},{10,11... | collective-permute-start | bytes 3932168 | tf_op jit(solution)/shard_map/ppermute | solution.py:37
  234.4 29.8 %collective-permute-start.13 = (bf16[1024,640]{1,0:T(8,128)(2,1)S(1)}, bf16[1024,640]{1,0:T(8,128)(2,1)S(1)}, u32[]{:S(2)}, u32[]{:S(2)}) collective-permute-start(bf16[1024,640]{1,0:T(8,128)(2,1)S(1)} %get-tuple-element.60), channel_id=1, source_target_pairs={{0,2},{1,3},{2,0},{3,1},{4,6},{5,7},{6,4},{7,5},{8,10},{9,11},{10,... | collective-permute-start | bytes 3932168 | tf_op jit(solution)/shard_map/ppermute | solution.py:37
  263.6 13.0 %collective-permute-start.14 = (bf16[512,640]{1,0:T(8,128)(2,1)}, bf16[512,640]{1,0:T(8,128)(2,1)S(1)}, u32[]{:S(2)}, u32[]{:S(2)}) collective-permute-start(bf16[512,640]{1,0:T(8,128)(2,1)} %slice.174), channel_id=1, source_target_pairs={{0,2},{1,3},{2,0},{3,1},{4,6},{5,7},{6,4},{7,5},{8,10},{9,11},{10,... | collective-permute-start | bytes 1966088 | tf_op jit(solution)/shard_map/ppermute | solution.py:37
  266.1 12.9 %collective-permute-start.15 = (bf16[512,640]{1,0:T(8,128)(2,1)}, bf16[512,640]{1,0:T(8,128)(2,1)}, u32[]{:S(2)}, u32[]{:S(2)}) collective-permute-start(bf16[512,640]{1,0:T(8,128)(2,1)} %slice.175), channel_id=1, source_target_pairs={{0,1},{1,0},{2,3},{3,2},{4,5},{5,4},{6,7},{7,6},{8,9},{9,8},{10,11... | collective-permute-start | bytes 1966088 | tf_op jit(solution)/shard_map/ppermute | solution.py:37
  395.4 8.5 collective-permute-start.42
  409.8 414.6 %reduce-scatter.12.cloned.1.call-start = ((), (), s32[]{:S(2)}) async-start(), calls=%async_computation.15 | async-start | bytes 6144000 | tf_op jit(solution)/shard_map/reduce_scatter | solution.py:373
  412.0 28.0 %copy-start.15 = (bf16[1024,1920]{1,0:T(8,128)(2,1)S(1)}, bf16[1024,1920]{1,0:T(8,128)(2,1)}, u32[]{:S(2)}) copy-start(bf16[1024,1920]{1,0:T(8,128)(2,1)} %get-tuple-element.63.up_ref.right_ref) | copy-start | bytes 11796484
  455.5 74.7 %collective-permute-start.43 = (bf16[1280,1920]{1,0:T(8,128)(2,1)}, bf16[1280,1920]{1,0:T(8,128)(2,1)}, u32[]{:S(2)}, u32[]{:S(2)}) collective-permute-start(bf16[1280,1920]{1,0:T(8,128)(2,1)} %get-tuple-element.53), channel_id=1, source_target_pairs={{0,4},{4,0},{8,12},{12,8},{16,20},{20,16},{24,28},{28,24},{1,5},{5... | collective-permute-start | bytes 14745608 | tf_op jit(solution)/shard_map/ppermute | solution.py:370
  456.1 31.0 %collective-permute-start.16 = (bf16[2,512,640]{2,1,0:T(8,128)(2,1)S(1)}, bf16[2,512,640]{2,1,0:T(8,128)(2,1)S(1)}, u32[]{:S(2)}, u32[]{:S(2)}) collective-permute-start(bf16[2,512,640]{2,1,0:T(8,128)(2,1)S(1)} %pad_maximum_fusion.4), channel_id=1, source_target_pairs={{0,1},{1,0},{2,3},{3,2},{4,5},{5,4},{6,7},{7,6},{8,9},{9,8},{10,11... | collective-permute-start | bytes 3932168 | tf_op jit(solution)/shard_map/ppermute | solution.py:37
  457.7 31.0 %collective-permute-start.18 = (bf16[2,512,640]{2,1,0:T(8,128)(2,1)S(1)}, bf16[2,512,640]{2,1,0:T(8,128)(2,1)S(1)}, u32[]{:S(2)}, u32[]{:S(2)}) collective-permute-start(bf16[2,512,640]{2,1,0:T(8,128)(2,1)S(1)} %pad_maximum_fusion.5), channel_id=1, source_target_pairs={{0,2},{1,3},{2,0},{3,1},{4,6},{5,7},{6,4},{7,5},{8,10},{9,11},{10,... | collective-permute-start | bytes 3932168 | tf_op jit(solution)/shard_map/ppermute | solution.py:37
  487.3 16.2 %collective-permute-start.17 = (bf16[512,640]{1,0:T(8,128)(2,1)S(1)}, bf16[512,640]{1,0:T(8,128)(2,1)S(1)}, u32[]{:S(2)}, u32[]{:S(2)}) collective-permute-start(bf16[512,640]{1,0:T(8,128)(2,1)S(1)} %fusion.38), channel_id=1, source_target_pairs={{0,2},{1,3},{2,0},{3,1},{4,6},{5,7},{6,4},{7,5},{8,10},{9,11},{10,... | collective-permute-start | bytes 1966088 | tf_op jit(solution)/shard_map/ppermute | solution.py:37
  504.1 19.1 %collective-permute-start.19 = (bf16[512,640]{1,0:T(8,128)(2,1)S(1)}, bf16[512,640]{1,0:T(8,128)(2,1)S(1)}, u32[]{:S(2)}, u32[]{:S(2)}) collective-permute-start(bf16[512,640]{1,0:T(8,128)(2,1)S(1)} %get-tuple-element.77), channel_id=1, source_target_pairs={{0,1},{1,0},{2,3},{3,2},{4,5},{5,4},{6,7},{7,6},{8,9},{9,8},{10,11... | collective-permute-start | bytes 1966088 | tf_op jit(solution)/shard_map/ppermute | solution.py:37
  505.3 14.2 %collective-permute-start.20 = (f32[8,128]{1,0:T(8,128)S(1)}, f32[8,128]{1,0:T(8,128)S(1)}, u32[]{:S(2)}, u32[]{:S(2)}) collective-permute-start(f32[8,128]{1,0:T(8,128)S(1)} %bitcast.215), channel_id=1, source_target_pairs={{0,1},{1,0},{2,3},{3,2},{4,5},{5,4},{6,7},{7,6},{8,9},{9,8},{10,11... | collective-permute-start | bytes 12296 | tf_op jit(solution)/shard_map/ppermute | solution.py:37
  519.5 3.6 collective-permute-start.21
  527.5 27.6 %collective-permute-start.26 = (bf16[1024,640]{1,0:T(8,128)(2,1)}, bf16[1024,640]{1,0:T(8,128)(2,1)S(1)}, u32[]{:S(2)}, u32[]{:S(2)}) collective-permute-start(bf16[1024,640]{1,0:T(8,128)(2,1)} %get-tuple-element.39), channel_id=1, source_target_pairs={{0,1},{1,0},{2,3},{3,2},{4,5},{5,4},{6,7},{7,6},{8,9},{9,8},{10,11... | collective-permute-start | bytes 3932168 | tf_op jit(solution)/shard_map/ppermute | solution.py:37
  528.7 29.5 %collective-permute-start.27 = (bf16[1024,640]{1,0:T(8,128)(2,1)}, bf16[1024,640]{1,0:T(8,128)(2,1)}, u32[]{:S(2)}, u32[]{:S(2)}) collective-permute-start(bf16[1024,640]{1,0:T(8,128)(2,1)} %get-tuple-element.39), channel_id=1, source_target_pairs={{0,2},{1,3},{2,0},{3,1},{4,6},{5,7},{6,4},{7,5},{8,10},{9,11},{10,... | collective-permute-start | bytes 3932168 | tf_op jit(solution)/shard_map/ppermute | solution.py:37
  555.2 25.5 %collective-permute-start.28 = (bf16[512,640]{1,0:T(8,128)(2,1)S(1)}, bf16[512,640]{1,0:T(8,128)(2,1)S(1)}, u32[]{:S(2)}, u32[]{:S(2)}) collective-permute-start(bf16[512,640]{1,0:T(8,128)(2,1)S(1)} %slice.186), channel_id=1, source_target_pairs={{0,2},{1,3},{2,0},{3,1},{4,6},{5,7},{6,4},{7,5},{8,10},{9,11},{10,... | collective-permute-start | bytes 1966088 | tf_op jit(solution)/shard_map/ppermute | solution.py:37
  559.3 21.5 %collective-permute-start.29 = (bf16[512,640]{1,0:T(8,128)(2,1)S(1)}, bf16[512,640]{1,0:T(8,128)(2,1)S(1)}, u32[]{:S(2)}, u32[]{:S(2)}) collective-permute-start(bf16[512,640]{1,0:T(8,128)(2,1)S(1)} %slice.187), channel_id=1, source_target_pairs={{0,1},{1,0},{2,3},{3,2},{4,5},{5,4},{6,7},{7,6},{8,9},{9,8},{10,11... | collective-permute-start | bytes 1966088 | tf_op jit(solution)/shard_map/ppermute | solution.py:37
  590.0 15.5 %all-to-all-start.2 = ((bf16[4,256,640]{2,1,0:T(8,128)(2,1)}), bf16[4,256,640]{2,1,0:T(8,128)(2,1)}, u32[]{:S(2)}, u32[]{:S(2)}) async-start(bf16[4,256,640]{2,1,0:T(8,128)(2,1)} %bitcast.212), calls=%async_computation.2 | async-start | bytes 2621440 | tf_op jit(solution)/shard_map/all_to_all | solution.py:111
  594.5 236.3 %reduce-scatter.6.cloned.1.call-start = ((), (), s32[]{:S(2)}) async-start(), calls=%async_computation.12 | async-start | bytes 4423680 | tf_op jit(solution)/shard_map/reduce_scatter | solution.py:364
  624.7 7.7 collective-permute-start.30
  626.2 7.8 collective-permute-start.32
  632.4 5.0 collective-permute-start.31
  637.5 6.4 collective-permute-start.33
  669.3 164.7 %reduce-scatter.8.cloned.1.call-start = ((), (), s32[]{:S(2)}) async-start(), calls=%async_computation.13 | async-start | bytes 3686400 | tf_op jit(solution)/shard_map/reduce_scatter | solution.py:364
  670.0 175.0 %reduce-scatter.14.cloned.1.call-start = ((), (), s32[]{:S(2)}) async-start(), calls=%async_computation.16 | async-start | bytes 6144000 | tf_op jit(solution)/shard_map/reduce_scatter | solution.py:373
  687.8 8.8 %collective-permute-start.46 = (bf16[1280,1920]{1,0:T(8,128)(2,1)}, bf16[1280,1920]{1,0:T(8,128)(2,1)S(1)}, u32[]{:S(2)}, u32[]{:S(2)}) collective-permute-start(bf16[1280,1920]{1,0:T(8,128)(2,1)} %get-tuple-element.56), channel_id=1, source_target_pairs={{0,4},{4,0},{8,12},{12,8},{16,20},{20,16},{24,28},{28,24},{1,5},{5... | collective-permute-start | bytes 14745608 | tf_op jit(solution)/shard_map/ppermute | solution.py:370
  704.6 31.7 %collective-permute-start.22 = (bf16[2,512,640]{2,1,0:T(8,128)(2,1)S(1)}, bf16[2,512,640]{2,1,0:T(8,128)(2,1)S(1)}, u32[]{:S(2)}, u32[]{:S(2)}) collective-permute-start(bf16[2,512,640]{2,1,0:T(8,128)(2,1)S(1)} %pad_maximum_fusion.6), channel_id=1, source_target_pairs={{0,1},{1,0},{2,3},{3,2},{4,5},{5,4},{6,7},{7,6},{8,9},{9,8},{10,11... | collective-permute-start | bytes 3932168 | tf_op jit(solution)/shard_map/ppermute | solution.py:37
  712.5 51.2 %copy-start.33 = (bf16[1024,2560]{1,0:T(8,128)(2,1)}, bf16[1024,2560]{1,0:T(8,128)(2,1)S(1)}, u32[]{:S(2)}) copy-start(bf16[1024,2560]{1,0:T(8,128)(2,1)S(1)} %convolution_convert_fusion.2) | copy-start | bytes 15728644
  712.9 50.8 %collective-permute-start.34 = (bf16[2,512,640]{2,1,0:T(8,128)(2,1)S(1)}, bf16[2,512,640]{2,1,0:T(8,128)(2,1)S(1)}, u32[]{:S(2)}, u32[]{:S(2)}) collective-permute-start(bf16[2,512,640]{2,1,0:T(8,128)(2,1)S(1)} %pad_maximum_fusion.8), channel_id=1, source_target_pairs={{0,1},{1,0},{2,3},{3,2},{4,5},{5,4},{6,7},{7,6},{8,9},{9,8},{10,11... | collective-permute-start | bytes 3932168 | tf_op jit(solution)/shard_map/ppermute | solution.py:37
  714.0 52.5 %collective-permute-start.24 = (bf16[2,512,640]{2,1,0:T(8,128)(2,1)S(1)}, bf16[2,512,640]{2,1,0:T(8,128)(2,1)}, u32[]{:S(2)}, u32[]{:S(2)}) collective-permute-start(bf16[2,512,640]{2,1,0:T(8,128)(2,1)S(1)} %pad_maximum_fusion.7), channel_id=1, source_target_pairs={{0,2},{1,3},{2,0},{3,1},{4,6},{5,7},{6,4},{7,5},{8,10},{9,11},{10,... | collective-permute-start | bytes 3932168 | tf_op jit(solution)/shard_map/ppermute | solution.py:37
  716.4 49.4 %copy-start.53 = (bf16[320]{0:T(512)(128)(2,1)S(1)}, bf16[320]{0:T(512)(128)(2,1)}, u32[]{:S(2)}) copy-start(bf16[320]{0:T(512)(128)(2,1)} %param.15) | copy-start | bytes 1924
  716.4 77.3 %collective-permute-start.36 = (bf16[2,512,640]{2,1,0:T(8,128)(2,1)}, bf16[2,512,640]{2,1,0:T(8,128)(2,1)}, u32[]{:S(2)}, u32[]{:S(2)}) collective-permute-start(bf16[2,512,640]{2,1,0:T(8,128)(2,1)} %pad_maximum_fusion.9), channel_id=1, source_target_pairs={{0,2},{1,3},{2,0},{3,1},{4,6},{5,7},{6,4},{7,5},{8,10},{9,11},{10,... | collective-permute-start | bytes 3932168 | tf_op jit(solution)/shard_map/ppermute | solution.py:37
  736.4 27.5 %copy-start.46 = (bf16[2,512,640]{2,1,0:T(8,128)(2,1)}, bf16[2,512,640]{2,1,0:T(8,128)(2,1)S(1)}, u32[]{:S(2)}) copy-start(bf16[2,512,640]{2,1,0:T(8,128)(2,1)S(1)} %collective-permute-done.22) | copy-start | bytes 3932164
  738.9 49.0 %collective-permute-start.23 = (bf16[512,640]{1,0:T(8,128)(2,1)}, bf16[512,640]{1,0:T(8,128)(2,1)}, u32[]{:S(2)}, u32[]{:S(2)}) collective-permute-start(bf16[512,640]{1,0:T(8,128)(2,1)} %fusion.34), channel_id=1, source_target_pairs={{0,2},{1,3},{2,0},{3,1},{4,6},{5,7},{6,4},{7,5},{8,10},{9,11},{10,... | collective-permute-start | bytes 1966088 | tf_op jit(solution)/shard_map/ppermute | solution.py:37
  764.7 35.9 %collective-permute-start.35 = (bf16[512,640]{1,0:T(8,128)(2,1)S(1)}, bf16[512,640]{1,0:T(8,128)(2,1)}, u32[]{:S(2)}, u32[]{:S(2)}) collective-permute-start(bf16[512,640]{1,0:T(8,128)(2,1)S(1)} %fusion.30), channel_id=1, source_target_pairs={{0,2},{1,3},{2,0},{3,1},{4,6},{5,7},{6,4},{7,5},{8,10},{9,11},{10,... | collective-permute-start | bytes 1966088 | tf_op jit(solution)/shard_map/ppermute | solution.py:37
  791.0 15.7 %collective-permute-start.25 = (bf16[512,640]{1,0:T(8,128)(2,1)}, bf16[512,640]{1,0:T(8,128)(2,1)}, u32[]{:S(2)}, u32[]{:S(2)}) collective-permute-start(bf16[512,640]{1,0:T(8,128)(2,1)} %get-tuple-element.71), channel_id=1, source_target_pairs={{0,1},{1,0},{2,3},{3,2},{4,5},{5,4},{6,7},{7,6},{8,9},{9,8},{10,11... | collective-permute-start | bytes 1966088 | tf_op jit(solution)/shard_map/ppermute | solution.py:37
  792.7 12.7 %collective-permute-start.38 = (f32[4,256]{1,0:T(4,128)S(1)}, f32[4,256]{1,0:T(4,128)S(1)}, u32[]{:S(2)}, u32[]{:S(2)}) collective-permute-start(f32[4,256]{1,0:T(4,128)S(1)} %dynamic_update_slice.85), channel_id=1, source_target_pairs={{0,1},{1,0},{2,3},{3,2},{4,5},{5,4},{6,7},{7,6},{8,9},{9,8},{10,11... | collective-permute-start | bytes 12296 | tf_op jit(solution)/shard_map/ppermute | solution.py:37
  803.7 15.7 %collective-permute-start.37 = (bf16[512,640]{1,0:T(8,128)(2,1)}, bf16[512,640]{1,0:T(8,128)(2,1)S(1)}, u32[]{:S(2)}, u32[]{:S(2)}) collective-permute-start(bf16[512,640]{1,0:T(8,128)(2,1)} %get-tuple-element.65), channel_id=1, source_target_pairs={{0,1},{1,0},{2,3},{3,2},{4,5},{5,4},{6,7},{7,6},{8,9},{9,8},{10,11... | collective-permute-start | bytes 1966088 | tf_op jit(solution)/shard_map/ppermute | solution.py:37
  805.5 3.7 collective-permute-start.39
  829.8 6.2 collective-permute-start.44
  833.0 4.0 collective-permute-start.40
  835.9 12.1 %collective-permute-start.45 = (f32[320]{0:T(512)S(1)}, f32[320]{0:T(512)S(1)}, u32[]{:S(2)}, u32[]{:S(2)}) collective-permute-start(f32[320]{0:T(512)S(1)} %add.379), channel_id=1, source_target_pairs={{0,2},{1,3},{2,0},{3,1},{4,6},{5,7},{6,4},{7,5},{8,10},{9,11},{10,... | collective-permute-start | bytes 3848 | tf_op jit(solution)/shard_map/ppermute | solution.py:37
  837.1 11.5 %collective-permute-start.41 = (f32[320]{0:T(512)S(1)}, f32[320]{0:T(512)S(1)}, u32[]{:S(2)}, u32[]{:S(2)}) collective-permute-start(f32[320]{0:T(512)S(1)} %add.374), channel_id=1, source_target_pairs={{0,2},{1,3},{2,0},{3,1},{4,6},{5,7},{6,4},{7,5},{8,10},{9,11},{10,... | collective-permute-start | bytes 3848 | tf_op jit(solution)/shard_map/ppermute | solution.py:37
  (51 other events, 487.0 us)
Sparse Core Ops, SparseCore 0:
  11.4 74.9 all-gather.3
  88.7 173.2 all-gather.5
  263.6 92.1 all-gather.7
  409.9 86.8 reduce-scatter.9
  536.4 84.9 reduce-scatter.11
  669.4 44.1 reduce-scatter.5
  715.9 39.4 reduce-scatter.7
  757.7 87.3 reduce-scatter.13

commit v3 on v2

--- a/solution.py
+++ b/solution.py
@@ -1,3 +1,4 @@
+import functools
 import math
 
 import jax
@@ -98,11 +99,57 @@
     )
 
 
+def gather_pieces(block):
+    half = block.shape[0] // 2
+    along_x = swap(block, 1)
+    along_y = swap(block, 2)
+    top = swap(along_x[:half], 2)
+    bottom = swap(along_y[half:], 1)
+    return block, along_x, along_y, top, bottom
+
+
+def assemble(pieces):
+    me = lax.axis_index("mdl")
+    own, along_x, along_y, top, bottom = pieces
+    rows, width = own.shape
+    whole = jnp.zeros((rows, 4 * width), own.dtype)
+    for piece, source, row in (
+        (own, me, 0),
+        (along_x, me ^ 1, 0),
+        (along_y, me ^ 2, 0),
+        (top, me ^ 3, 0),
+        (bottom, me ^ 3, rows // 2),
+    ):
+        whole = lax.dynamic_update_slice(whole, piece, (row, source * width))
+    return whole
+
+
+def scatter_payload(payload):
+    top_sent, bottom_sent, top_kept, bottom_kept = payload
+    got_top = swap(top_sent, 1)
+    got_bottom = swap(bottom_sent, 2)
+    halves = []
+    for kept, got, second in ((top_kept, got_top, 2), (bottom_kept, got_bottom, 1)):
+        passed = (kept[1].astype(F32) + got[1].astype(F32)).astype(BF16)
+        last = swap(passed, second)
+        halves.append(kept[0].astype(F32) + got[0].astype(F32) + last.astype(F32))
+    return jnp.concatenate(halves, axis=0)
+
+
 def sum_mdl(value):
     size = lax.axis_size("mdl")
     distance = 1
     while distance < size:
         value = value + swap(value, distance)
+        distance *= 2
+    return value
+
+
+def sum_tok(value):
+    size = lax.axis_size("tok")
+    distance = 1
+    while distance < size:
+        value = value + lax.ppermute(value, "tok", [(i, i ^ distance) for i in range(size)])
         distance *= 2
     return value
 
@@ -256,6 +303,15 @@
         sent_ref[...] = total[:half]
 
 
+def split_pairs(total, pairs, core):
+    rows, cols = total.shape
+    total = total.reshape(pairs, 2, rows // pairs // 2, cols)
+    return tuple(
+        lax.dynamic_index_in_dim(total, index, 1, False).reshape(-1, cols)
+        for index in (core, 1 - core)
+    )
+
+
 def pair_grad(left, right):
     tokens, rows = left.shape
     cols = right.shape[1]
@@ -263,12 +319,7 @@
     core = lax.axis_index("tok") % 2
     step = rows // pairs
     if step % 128:
-        total = tn(left, right).astype(BF16).reshape(pairs, 2, step // 2, cols)
-        kept, sent = (
-            lax.dynamic_index_in_dim(total, index, 1, False).reshape(-1, cols)
-            for index in (core, 1 - core)
-        )
-        return kept, sent
+        return split_pairs(tn(left, right).astype(BF16), pairs, core)
     out = jax.ShapeDtypeStruct((rows // 2, cols), BF16)
     out_spec = pl.BlockSpec((step // 2, cols), lambda pair: (pair, 0))
     return pl.pallas_call(
@@ -293,36 +344,170 @@
     )(core.astype(jnp.int32).reshape(1), left, right)
 
 
-def two_kernel(gate_ref, up_ref, weight_ref, out_ref):
-    cols = gate_ref.shape[1]
-    out_ref[...] = (
-        nt(gate_ref[...], weight_ref[:, :cols]) + nt(up_ref[...], weight_ref[:, cols:])
-    ).astype(BF16)
-
-
-def two_products(d_gate, d_up, weight):
-    tokens, cols = d_gate.shape
-    rows = weight.shape[0]
-    if cols % 128:
-        return (nt(d_gate, weight[:, :cols]) + nt(d_up, weight[:, cols:])).astype(BF16)
-    step = 512
-    whole = pl.BlockSpec((tokens, cols), lambda row: (0, 0))
+def payload_kernel(starts, me_ref, *refs):
+    lefts, weight_ref = refs[: len(starts)], refs[len(starts)]
+    top_sent, bottom_sent, top_kept, bottom_kept = refs[len(starts) + 1 :]
+    total = 0.0
+    for left_ref, start in zip(lefts, starts):
+        total += nt(left_ref[...], weight_ref[:, start : start + left_ref.shape[1]])
+    total = total.astype(BF16)
+    half = total.shape[0] // 2
+    places = (
+        ((top_kept, 0), (bottom_kept, 0)),
+        ((top_sent, 0), (bottom_kept, 1)),
+        ((top_kept, 1), (bottom_sent, 0)),
+        ((top_sent, 1), (bottom_sent, 1)),
+    )
+    for distance, ((top, top_at), (bottom, bottom_at)) in enumerate(places):
+
+        @pl.when(pl.program_id(0) == 3 - distance)
+        def _(top=top, top_at=top_at, bottom=bottom, bottom_at=bottom_at):
+            top[top_at] = total[:half]
+            bottom[bottom_at] = total[half:]
+
+
+def scatter_product(lefts, weight, starts):
+    tokens = lefts[0].shape[0]
+    rows, cols = weight.shape
+    step = rows // 4
+    me = lax.axis_index("mdl").astype(jnp.int32).reshape(1)
+    out = jax.ShapeDtypeStruct((2, tokens // 2, step), BF16)
+    depth = sum(left.shape[1] for left in lefts)
     return pl.pallas_call(
-        two_kernel,
-        grid=(rows // step,),
-        out_shape=jax.ShapeDtypeStruct((tokens, rows), BF16),
-        in_specs=[whole, whole, pl.BlockSpec((step, 2 * cols), lambda row: (row, 0))],
-        out_specs=pl.BlockSpec((tokens, step), lambda row: (0, row)),
+        functools.partial(payload_kernel, starts),
+        grid_spec=pltpu.PrefetchScalarGridSpec(
+            num_scalar_prefetch=1,
+            grid=(4,),
+            in_specs=[pl.BlockSpec(left.shape, lambda at, me_ref: (0, 0)) for left in lefts]
+            + [pl.BlockSpec((step, cols), lambda at, me_ref: (me_ref[0] ^ (3 - at), 0))],
+            out_specs=[pl.BlockSpec(out.shape, lambda at, me_ref: (0, 0, 0))] * 4,
+        ),
+        out_shape=(out,) * 4,
         compiler_params=pltpu.CompilerParams(
             dimension_semantics=("arbitrary",), vmem_limit_bytes=48 << 20
         ),
         cost_estimate=pl.CostEstimate(
-            flops=4 * tokens * rows * cols,
-            bytes_accessed=4 * tokens * cols + 4 * rows * cols + 2 * tokens * rows,
+            flops=2 * tokens * rows * depth,
+            bytes_accessed=2 * (tokens * depth + rows * cols + tokens * rows),
             transcendentals=0,
         ),
-        name="two_products",
-    )(d_gate, d_up, weight)
+        name="scatter_product",
+    )(me, *lefts, weight)
+
+
+def pieces_kernel(start, me_ref, own, along_x, along_y, top, bottom, weight_ref, out_ref, total):
+    at = pl.program_id(0)
+    width = out_ref.shape[1]
+    half = top.shape[0]
+    for index, piece in enumerate((own, along_x, along_y)):
+
+        @pl.when(at == index)
+        def _(index=index, piece=piece):
+            part = nn(piece[...], weight_ref[:, start : start + width])
+            if index:
+                total[...] += part
+            else:
+                total[...] = part
+
+    @pl.when(at == 3)
+    def _():
+        weight = weight_ref[:, start : start + width]
+        out_ref[:half] = (total[:half] + nn(top[...], weight)).astype(BF16)
+        out_ref[half:] = (total[half:] + nn(bottom[...], weight)).astype(BF16)
+
+
+def pieces_product(pieces, weight, start, width):
+    tokens, step = pieces[0].shape
+    rows, cols = weight.shape
+    me = lax.axis_index("mdl").astype(jnp.int32).reshape(1)
+    return pl.pallas_call(
+        functools.partial(pieces_kernel, start),
+        grid_spec=pltpu.PrefetchScalarGridSpec(
+            num_scalar_prefetch=1,
+            grid=(4,),
+            in_specs=[pl.BlockSpec(piece.shape, lambda at, me_ref: (0, 0)) for piece in pieces]
+            + [pl.BlockSpec((step, cols), lambda at, me_ref: (me_ref[0] ^ at, 0))],
+            out_specs=pl.BlockSpec((tokens, width), lambda at, me_ref: (0, 0)),
+            scratch_shapes=[pltpu.VMEM((tokens, width), F32)],
+        ),
+        out_shape=jax.ShapeDtypeStruct((tokens, width), BF16),
+        compiler_params=pltpu.CompilerParams(
+            dimension_semantics=("arbitrary",), vmem_limit_bytes=40 << 20
+        ),
+        cost_estimate=pl.CostEstimate(
+            flops=2 * tokens * rows * width,
+            bytes_accessed=2 * (tokens * rows + rows * cols + tokens * width),
+            transcendentals=0,
+        ),
+        name="pieces_product",
+    )(me, *pieces, weight)
+
+
+def attn_kernel(core_ref, rows_ref, d_qkv_ref, mixed_ref, heads_ref, weight_ref, kept, sent, gain):
+    cols = d_qkv_ref.shape[1]
+    d_weight = tn(rows_ref[...], d_qkv_ref[...])
+    gain[...] = jnp.sum(d_weight * weight_ref[:, :cols].astype(F32), axis=1, keepdims=True)
+    left = d_weight.astype(BF16)
+    right = tn(mixed_ref[...], heads_ref[...]).astype(BF16)
+    half = left.shape[0] // 2
+    for core, (first, second) in enumerate(((kept, sent), (sent, kept))):
+
+        @pl.when(core_ref[0] == core)
+        def _(first=first, second=second):
+            first[:, :cols] = left[:half]
+            first[:, cols:] = right[:half]
+            second[:, :cols] = left[half:]
+            second[:, cols:] = right[half:]
+
+
+def attn_grad(rows_in, d_qkv, d_mixed, head_block, weight):
+    tokens, rows = rows_in.shape
+    qkv_cols, cols = d_qkv.shape[1], weight.shape[1]
+    pairs = lax.axis_size("tok") // 2
+    core = lax.axis_index("tok") % 2
+    step = rows // pairs
+    if step % 128 or qkv_cols % 128:
+        d_weight = tn(rows_in, d_qkv)
+        gain = jnp.sum(d_weight * weight[:, :qkv_cols].astype(F32), axis=1, keepdims=True)
+        total = jnp.concatenate([d_weight, tn(d_mixed, head_block)], axis=1).astype(BF16)
+        return split_pairs(total, pairs, core), gain
+    out = jax.ShapeDtypeStruct((rows // 2, cols), BF16)
+    out_spec = pl.BlockSpec((step // 2, cols), lambda pair: (pair, 0))
+    left_spec = pl.BlockSpec((tokens, step), lambda pair: (0, pair))
+    kept, sent, gain = pl.pallas_call(
+        attn_kernel,
+        grid=(pairs,),
+        out_shape=(out, out, jax.ShapeDtypeStruct((rows, 1), F32)),
+        in_specs=[
+            pl.BlockSpec(memory_space=pltpu.SMEM),
+            left_spec,
+            pl.BlockSpec(d_qkv.shape, lambda pair: (0, 0)),
+            left_spec,
+            pl.BlockSpec(head_block.shape, lambda pair: (0, 0)),
+            pl.BlockSpec((step, cols), lambda pair: (pair, 0)),
+        ],
+        out_specs=(out_spec, out_spec, pl.BlockSpec((step, 1), lambda pair: (pair, 0))),
+        compiler_params=pltpu.CompilerParams(
+            dimension_semantics=("arbitrary",), vmem_limit_bytes=40 << 20
+        ),
+        cost_estimate=pl.CostEstimate(
+            flops=2 * tokens * rows * cols,
+            bytes_accessed=4 * tokens * rows + 2 * tokens * cols + 4 * rows * cols,
+            transcendentals=0,
+        ),
+        name="attn_grad",
+    )(core.astype(jnp.int32).reshape(1), rows_in, d_qkv, d_mixed, head_block, weight)
+    return (kept, sent), gain
+
+
+def product_to_mdl(lefts, weight, starts):
+    if lax.axis_size("mdl") == 4:
+        payload = scatter_product(lefts, weight, starts)
+        return payload, lambda payload: scatter_payload(payload)
+    part = sum(
+        nt(left, weight[:, start : start + left.shape[1]]) for left, start in zip(lefts, starts)
+    )
+    return (part.astype(BF16),), lambda payload: scatter_mdl(payload[0], 1)
 
 
 def after(value, *earlier):
@@ -359,10 +544,6 @@
 
     def from_tok(weight, dim):
         return lax.all_gather(weight, "tok", axis=dim, tiled=True)
-
-    def to_tok(grad, dim):
-        total = lax.psum_scatter(grad, "tok", scatter_dimension=dim, tiled=True)
-        return total.astype(F32)
 
     def pair_to_tok(local):
         kept, sent = local
@@ -376,11 +557,12 @@
         return total.astype(F32)
 
     qkv_cols, ff_cols = qkv_weight.shape[1], gate_weight.shape[1]
-    w_attn = from_tok(jnp.concatenate([scaled(qkv_weight, norm1_gain), out_weight.T], axis=1), 0)
-    w_qkv, w_out_t = w_attn[:, :qkv_cols], w_attn[:, qkv_cols:]
+    attn_local = jnp.concatenate([scaled(qkv_weight, norm1_gain), out_weight.T], axis=1)
+    w_attn = from_tok(attn_local, 0)
+    w_qkv = w_attn[:, :qkv_cols]
     gu_local = jnp.concatenate([scaled(w, norm2_gain) for w in (gate_weight, up_weight)], 1)
     w_gu = from_tok(gu_local, 0)
-    w_down = from_tok(down_weight, 1)
+    w_down_t = from_tok(down_weight.T, 0)
 
     rows_in = gather_mdl(inputs, 1)
     scale_one = row_scale(rows_in)
@@ -398,7 +580,8 @@
     attended, log_norm = attention_forward(first, qkv, kv, cos, sin, pos)
     head_block = cols_to_rows(attended)
     residual = inputs.astype(F32)
-    mixed = residual + scatter_mdl(nt(head_block, w_out_t).astype(BF16), 1)
+    payload, scatter = product_to_mdl((head_block,), w_attn, (qkv_cols,))
+    mixed = residual + scatter(payload)
 
     rows_two = gather_mdl(mixed.astype(BF16), 1)
     scale_two = row_scale(rows_two)
@@ -412,33 +595,36 @@
 
     down_local = pair_grad(cotangent, hidden)
     down_grad = pair_to_tok(down_local).T
-    d_hidden = nt(cotangent, w_down)
+    d_hidden = nn(cotangent, w_down_t)
     d_gate_f = d_hidden * up_in * slope
     d_up_f = d_hidden * gelu
     stat_two = jnp.sum(d_gate_f * gate_in + d_up_f * up_in, axis=1)
     d_gate, d_up = d_gate_f.astype(BF16), d_up_f.astype(BF16)
     gate_local = pair_grad(rows_hat, d_gate)
     gate_sum = pair_to_tok(gate_local)
-    d_two_part = two_products(d_gate, d_up, w_gu)
-    rows_later = after(rows_hat, d_two_part)
+    payload, scatter = product_to_mdl((d_gate, d_up), w_gu, (0, ff_cols))
+    rows_later = after(rows_hat, payload[0])
     up_local = pair_grad(rows_later, d_up)
     up_sum = pair_to_tok(up_local)
-    d_two = scatter_mdl(d_two_part, 1)
+    d_two = scatter(payload)
     stat_two = sum_mdl(stat_two.reshape(8, -1)).reshape(-1, 1) * (1.0 / features)
     scale_mixed = scale_two * mixed
     cotangent_own = lax.dynamic_slice_in_dim(cotangent, me * width, width, 1).astype(F32)
     d_mixed = cotangent_own + scale_two * (d_two - scale_mixed * stat_two)
 
     d_mixed_b = after(d_mixed.astype(BF16), up_local[0])
-    d_mixed_rows = gather_mdl(d_mixed_b, 1)
     hidden_later = after(hidden, d_mixed_b)
-    ffn_part = nn(hidden_later, w_down).astype(BF16)
-    d_head = nn(after(d_mixed_rows, ffn_part), w_out_t).astype(BF16)
+    ffn_payload, ffn_scatter = product_to_mdl((hidden_later,), w_down_t, (0,))
+    out_cols = head_block.shape[1]
+    if size == 4:
+        pieces = gather_pieces(d_mixed_b)
+        d_head = pieces_product(pieces, w_attn, qkv_cols, out_cols)
+        d_mixed_rows = assemble(tuple(after(piece, d_head) for piece in pieces))
+    else:
+        d_mixed_rows = gather_mdl(d_mixed_b, 1)
+        d_head = nn(d_mixed_rows, w_attn[:, qkv_cols:]).astype(BF16)
     d_attended = rows_to_cols(d_head)
-    out_local = tn(d_mixed_rows, after(head_block, d_head)).astype(BF16)
-    out_grad = to_tok(out_local, 0).T
-    d_attended = after(d_attended, out_local)
-    block_out = (mixed + scatter_mdl(ffn_part, 1)).astype(BF16)
+    block_out = (mixed + ffn_scatter(ffn_payload)).astype(BF16)
     d_query, d_kv = attention_backward(
         first, qkv, kv, cos, sin, pos, attended, d_attended, log_norm
     )
@@ -450,23 +636,31 @@
     stat_rows = jnp.zeros((size, count), F32)
     stat_rows = sum_mdl(lax.dynamic_update_slice(stat_rows, stat_one[None], (me, 0)))
     stat_one = stat_rows.reshape(-1, 1) * (1.0 / features)
-    qkv_local = tn(rows_in, (d_qkv_part.astype(F32) * scale_one).astype(BF16)).astype(BF16)
-    qkv_sum = to_tok(qkv_local, 0)
-    d_one = scatter_mdl(nt(d_qkv_part, w_qkv).astype(BF16), 1)
+    d_scaled = (d_qkv_part.astype(F32) * scale_one).astype(BF16)
+    attn_local, gain_one = attn_grad(rows_in, d_scaled, d_mixed_rows, head_block, w_attn)
+    attn_sum = pair_to_tok(attn_local)
+    qkv_sum, out_grad = attn_sum[:, :qkv_cols], attn_sum[:, qkv_cols:].T
+    d_later = after(d_qkv_part, attn_local[0])
+    payload, scatter = product_to_mdl((d_later,), w_attn, (0,))
+    d_one = scatter(payload)
     input_grad = d_mixed + scale_one * (d_one - (scale_one * residual) * stat_one)
 
-    norm1_late, norm2_late, qkv_late, gate_late, up_late, _ = lax.optimization_barrier(
-        (norm1_gain, norm2_gain, qkv_weight, gate_weight, up_weight, up_local[0])
+    norm1_late, norm2_late, gate_late, up_late, _ = lax.optimization_barrier(
+        (norm1_gain, norm2_gain, gate_weight, up_weight, up_local[0])
     )
 
     def unfold(total, gain):
         return total * gain.astype(F32)[:, None]
 
-    def gain_grad(*pairs):
-        return sum(jnp.sum(weight.astype(F32) * total, axis=1) for weight, total in pairs)
-
-    gain_two_grad = sum_mdl(gain_grad((gate_late, gate_sum), (up_late, up_sum)))
-    gain_one_grad = sum_mdl(gain_grad((qkv_late, qkv_sum)))
+    gain_two = jnp.sum(
+        gate_late.astype(F32) * gate_sum + up_late.astype(F32) * up_sum, axis=1
+    )
+    gate_grad, up_grad = unfold(gate_sum, norm2_late), unfold(up_sum, norm2_late)
+    gain_two_grad = sum_mdl(gain_two)
+    gain_one = sum_tok(sum_mdl(gain_one.reshape(8, -1))).reshape(-1)
+    shard = norm1_gain.shape[0]
+    gain_one = lax.dynamic_slice_in_dim(gain_one, lax.axis_index("tok") * shard, shard, 0)
+    gain_one_grad = gain_one / norm1_late.astype(F32)
     return (
         block_out,
         input_grad,
@@ -474,8 +668,8 @@
         unfold(qkv_sum, norm1_late),
         out_grad,
         gain_two_grad,
-        unfold(gate_sum, norm2_late),
-        unfold(up_sum, norm2_late),
+        gate_grad,
+        up_grad,
         down_grad,
     )
 

time: 865 us -> 875 us (1.012)
  matrix products: 125 us -> 68.9 us
  Pallas kernels: 102 us -> 158 us
  blocking collectives: 32.9 us -> 18.5 us
  other arithmetic: 77.5 us -> 90 us
  local copies, waits for them, and re-layouts: 38.9 us -> 50.7 us
    pallas_call x1 -> x6, Pallas kernels: 28 us -> 83.9 us  [the longest x4 66.4 us: scatter_product(): pl.pallas_call(functools.partial(payload_kernel, starts), grid_spec=pltpu...]
    dot_general x5 -> x0, matrix products: 54 us -> none  [the longest x3 36.5 us: nt(): lax.dot_general(left_op, right_op, (((1,), (1,)), ((), ())), preferred_el...]
    ppermute x44, waiting for transfers between devices: 309 us -> 274 us  [swap(): return lax.ppermute(block, 'mdl', [(i, i ^ distance) for i in range(size)])]
    all_to_all x2 -> x1, blocking collectives: 32.9 us -> 18.5 us  [cols_to_rows(): return lax.all_to_all(block, 'mdl', split_axis=1, concat_axis=0, tiled=True)]
    all_gather x3, waiting for transfers between devices: 45.7 us -> 58.8 us  [from_tok(): return lax.all_gather(weight, 'tok', axis=dim, tiled=True)]
    all_to_all x2, waiting for transfers between devices: 21.5 us -> 33.7 us  [rows_to_cols(): return lax.all_to_all(block, 'mdl', split_axis=0, concat_axis=1, tiled=True)]
    add x1 -> x11, other arithmetic: 0.01 us -> 11.2 us  [the longest x8 11.2 us: scatter_payload(): halves.append(kept[0].astype(F32) + got[0].astype(F32) + last.astype(F32))]
    convert_element_type x0 -> x11, other arithmetic: none -> 10.1 us  [the longest x8 7.07 us: scatter_payload(): passed = (kept[1].astype(F32) + got[1].astype(F32)).astype(BF16)]
  transfers between devices with their start and end apart: 57 -> 61, of which waited for: 36 -> 37; matrix products, arithmetic and copies ran while one was open for 23% -> 17% of each run, Pallas kernels for 10% -> 16%
where the time goes in v3:
time: 875 us; the launch traced here: 866 us
  waiting for transfers between devices  400 us (46%)
  Pallas kernels  158 us (18%)
  other arithmetic  90 us (10%)
  matrix products  68.9 us (8%)
  starting transfers between devices  64.2 us (7%)
  local copies, waits for them, and re-layouts  50.7 us (6%)
  blocking collectives  18.5 us (2%)
  between operations  15.4 us (2%)
    ppermute x44, waiting for transfers between devices, swap(): return lax.ppermute(block, 'mdl', [(i, i ^ distance) for i in range(size)])  274 us
    dot_general x4, matrix products, nn(): return jnp.dot(left_op, right_op, preferred_element_type=F32)  68.9 us
    pallas_call x4, Pallas kernels, scatter_product(): pl.pallas_call(functools.partial(payload_kernel, starts), grid_spec=pltpu...  66.4 us
    all_gather x3, waiting for transfers between devices, from_tok(): return lax.all_gather(weight, 'tok', axis=dim, tiled=True)  58.8 us
    ppermute x44, starting transfers between devices, swap(): return lax.ppermute(block, 'mdl', [(i, i ^ distance) for i in range(size)])  49.8 us
    pallas_call x3, Pallas kernels, pair_grad(): pl.pallas_call(pair_kernel, grid=(pairs,), out_shape=(out, out), in_specs...  47.6 us
    all_to_all x2, waiting for transfers between devices, rows_to_cols(): return lax.all_to_all(block, 'mdl', split_axis=0, concat_axis=1, tiled=True)  33.7 us
    ppermute x4, waiting for transfers between devices, pair_to_tok(): got = lax.ppermute(sent, 'tok', [(i, i ^ 1) for i in range(count)])  22.8 us
  transfers between devices with their start and end apart: 61, of which 37 were waited for; matrix products, arithmetic and copies ran while one was open for 17% of the time, Pallas kernels for 16%

profile of v3, /device:TPU:0, one launch (start us, length us, event | category | flops | bytes accessed | tf_op | source)
XLA Modules:
  0.0 866.0 jit_solution(13840580097110699591)
XLA Ops:
  13.8 3.0 collective-permute-start
  18.3 27.3 %collective-permute-done = bf16[1024,640]{1,0:T(8,128)(2,1)S(1)} collective-permute-done((bf16[1024,640]{1,0:T(8,128)(2,1)S(1)}, bf16[1024,640]{1,0:T(8,128)(2,1)S(1)}, u32[]{:S(2)}, u32[]{:S(2)}) %collective-permute-start) | collective-permute-done | bytes 1310752 | tf_op jit(solution)/shard_map/ppermute | solution.py:38
  53.6 9.0 %collective-permute-done.2 = bf16[512,640]{1,0:T(8,128)(2,1)S(1)} collective-permute-done((bf16[512,640]{1,0:T(8,128)(2,1)}, bf16[512,640]{1,0:T(8,128)(2,1)S(1)}, u32[]{:S(2)}, u32[]{:S(2)}) %collective-permute-start.2) | collective-permute-done | bytes 655392 | tf_op jit(solution)/shard_map/ppermute | solution.py:38
  62.7 3.2 collective-permute-done.3
  69.4 17.0 %all-gather.4.cloned.1.call-done.refs_1_.weight_ref = bf16[2560,1408]{1,0:T(8,128)(2,1)} async-done(((bf16[320,1408]{1,0:T(8,128)(2,1)}), bf16[2560,1408]{1,0:T(8,128)(2,1)}) %all-gather.4.cloned.1.call-update) | async-done | bytes 7208976 | tf_op jit(solution)/shard_map/all_gather | solution.py:546
  86.4 9.0 %multiply_convert_fusion.2 = bf16[1024,768]{1,0:T(8,128)(2,1)} fusion(bf16[1024,2560]{1,0:T(8,128)(2,1)} %copy-done.43, bf16[2560,1408]{1,0:T(8,128)(2,1)} %all-gather.4.cloned.1.call-done.refs_1_.weight_ref, f32[1024]{0:T(1024)S(1)} %add_rsqrt_fusion.1), kind=kOutput, calls=%fused_computation.27 | convolution fusion | flops 4028104704 | bytes 10752000 | tf_op jit(solution)/shard_map/dot_general | solution.py:33
  95.5 3.8 all-to-all-start
  99.3 19.8 %all-to-all-done = bf16[4,256,768]{2,1,0:T(8,128)(2,1)S(1)} async-done(((bf16[4,256,768]{2,1,0:T(8,128)(2,1)}), bf16[4,256,768]{2,1,0:T(8,128)(2,1)S(1)}, u32[]{:S(2)}, u32[]{:S(2)}) %all-to-all-start) | async-done | bytes 1572896 | tf_op jit(solution)/shard_map/all_to_all | solution.py:158
  123.9 5.7 collective-permute-done.4
  131.8 2.8 collective-permute-done.6
  136.2 10.8 %attention_forward.1 = (bf16[256,2560]{1,0:T(8,128)(2,1)S(1)}, f32[10,256,1]{2,1,0:T(8,128)S(1)}) custom-call(s32[1]{0:T(128)} %bitcast.1.first_ref, bf16[256,3072]{1,0:T(8,128)(2,1)S(1)} %bitcast.115, bf16[1024,512]{1,0:T(8,128)(2,1)S(1)} %constant_dynamic-update-slice_fusion.8.kv_ref, f32[256,128]{1,0:T(8,128)S(1)} %get-tuple-element.128.cos_ref, ...), custom_call_target="tpu_custom_call" | custom-call | flops 2684354560 | bytes 3670016 | tf_op jit(solution)/shard_map/attention_forward/pallas_call | solution.py:229
  147.2 18.5 %all_to_all.76 = bf16[256,4,640]{2,0,1:T(8,128)(2,1)} all-to-all(bf16[256,4,640]{2,0,1:T(8,128)(2,1)S(1)} %bitcast.125), channel_id=1, replica_groups=mesh['tok'=8,'mdl'=4] {'mdl'}, dimensions={1} | all-to-all | bytes 2621440 | tf_op jit(solution)/shard_map/all_to_all | solution.py:162
  165.7 7.8 scatter_product.4
  175.1 25.6 %collective-permute-done.8 = bf16[2,512,640]{2,1,0:T(8,128)(2,1)S(1)} collective-permute-done((bf16[2,512,640]{2,1,0:T(8,128)(2,1)S(1)}, bf16[2,512,640]{2,1,0:T(8,128)(2,1)S(1)}, u32[]{:S(2)}, u32[]{:S(2)}) %collective-permute-start.8) | collective-permute-done | bytes 1310752 | tf_op jit(solution)/shard_map/ppermute | solution.py:38
  204.4 11.3 %collective-permute-done.9 = bf16[512,640]{1,0:T(8,128)(2,1)S(1)} collective-permute-done((bf16[512,640]{1,0:T(8,128)(2,1)S(1)}, bf16[512,640]{1,0:T(8,128)(2,1)S(1)}, u32[]{:S(2)}, u32[]{:S(2)}) %collective-permute-start.9) | collective-permute-done | bytes 655392 | tf_op jit(solution)/shard_map/ppermute | solution.py:38
  216.2 2.6 broadcast.71.clone
  222.6 26.0 %collective-permute-done.12 = bf16[1024,640]{1,0:T(8,128)(2,1)S(1)} collective-permute-done((bf16[1024,640]{1,0:T(8,128)(2,1)S(1)}, bf16[1024,640]{1,0:T(8,128)(2,1)S(1)}, u32[]{:S(2)}, u32[]{:S(2)}) %collective-permute-start.12) | collective-permute-done | bytes 1310752 | tf_op jit(solution)/shard_map/ppermute | solution.py:38
  255.2 7.8 collective-permute-done.14
  266.5 3.8 fusion
  270.3 6.6 fusion.1.rows_ref
  277.0 17.4 %fusion.4 = f32[1024,1920]{1,0:T(8,128)} fusion(bf16[1024,2560]{1,0:T(8,128)(2,1)} %fusion.1.rows_ref, bf16[2560,3840]{1,0:T(8,128)(2,1)} %all-gather.6.cloned.1.call-done.refs_2_), kind=kOutput, calls=%fused_computation.7 | convolution fusion | flops 10066329600 | bytes 22937600 | tf_op jit(solution)/shard_map/dot_general | solution.py:33
  294.3 19.7 %multiply_convert_fusion = (bf16[1024,1920]{1,0:T(8,128)(2,1)}, f32[1024,1920]{1,0:T(8,128)}) fusion(f32[1024,1920]{1,0:T(8,128)} %fusion.4, bf16[1024,2560]{1,0:T(8,128)(2,1)S(1)} %copy-done.51, bf16[2560,3840]{1,0:T(8,128)(2,1)} %all-gather.6.cloned.1.call-done.refs_2_), kind=kOutput, calls=%fused_computation.18 | convolution fusion | flops 10085990400 | bytes 34734080 | tf_op jit(solution)/shard_map/dot_general | solution.py:33
  314.0 41.8 %all-gather.8.cloned.1.call-done.refs_1_ = bf16[2560,1920]{1,0:T(8,128)(2,1)} async-done(((bf16[320,1920]{1,0:T(8,128)(2,1)}), bf16[2560,1920]{1,0:T(8,128)(2,1)}) %all-gather.8.cloned.1.call-update) | async-done | bytes 9830416 | tf_op jit(solution)/shard_map/all_gather | solution.py:546
  355.8 22.8 %fusion.53 = (bf16[1024,1920]{1,0:T(8,128)(2,1)S(1)}, f32[1024]{0:T(1024)S(1)}, bf16[1024,1920]{1,0:T(8,128)(2,1)}) fusion(f32[1024,1920]{1,0:T(8,128)} %fusion.4, f32[1024,1920]{1,0:T(8,128)} %get-tuple-element.60, bf16[1024,2560]{1,0:T(8,128)(2,1)} %rows_ref.1, bf16[2560,1920]{1,0:T(8,128)(2,1)} %all-gather.8.cloned.1.call-done.refs_1_), kind=kOutput, calls=%fused_computation.154 | convolution fusion | flops 10117446656 | bytes 38670336 | tf_op jit(solution)/shard_map/dot_general | solution.py:33
  378.6 16.5 %pair_grad.4 = (bf16[1280,1920]{1,0:T(8,128)(2,1)}, bf16[1280,1920]{1,0:T(8,128)(2,1)}) custom-call(s32[1]{0:T(128)} %bitcast.19.core_ref, bf16[1024,2560]{1,0:T(8,128)(2,1)} %fusion.1.rows_ref, bf16[1024,1920]{1,0:T(8,128)(2,1)S(1)} %get-tuple-element.103.refs_0_.right_ref), custom_call_target="tpu_custom_call" | custom-call | flops 10066329600 | bytes 19005440 | tf_op jit(solution)/shard_map/pair_grad/pallas_call | solution.py:325
  395.4 8.2 collective-permute-done.46
  403.6 5.9 add_convert_fusion.2
  409.6 32.2 %scatter_product.5 = (bf16[2,512,640]{2,1,0:T(8,128)(2,1)S(1)}, bf16[2,512,640]{2,1,0:T(8,128)(2,1)S(1)}, bf16[2,512,640]{2,1,0:T(8,128)(2,1)S(1)}, bf16[2,512,640]{2,1,0:T(8,128)(2,1)S(1)}) custom-call(s32[1]{0:T(128)} %bitcast.me_ref, bf16[1024,1920]{1,0:T(8,128)(2,1)} %copy-done.32, bf16[1024,1920]{1,0:T(8,128)(2,1)} %get-tuple-element.105.refs_1_.right_ref, ...), custom_call_target="tpu_custom_call" | custom-call | flops 20132659200 | bytes 32768000 | tf_op jit(solution)/shard_map/scatter_product/pallas_call | solution.py:376
  443.9 15.5 %pair_grad.3 = (bf16[1280,1920]{1,0:T(8,128)(2,1)}, bf16[1280,1920]{1,0:T(8,128)(2,1)}) custom-call(s32[1]{0:T(128)} %bitcast.19.core_ref, bf16[1024,2560]{1,0:T(8,128)(2,1)} %fusion.1.rows_ref, bf16[1024,1920]{1,0:T(8,128)(2,1)S(1)} %copy-done.31), custom_call_target="tpu_custom_call" | custom-call | flops 10066329600 | bytes 19005440 | tf_op jit(solution)/shard_map/pair_grad/pallas_call | solution.py:325
  459.5 8.3 collective-permute-done.47
  467.8 5.9 add_convert_fusion.1
  478.7 15.6 %pair_grad.5 = (bf16[1280,1920]{1,0:T(8,128)(2,1)}, bf16[1280,1920]{1,0:T(8,128)(2,1)}) custom-call(s32[1]{0:T(128)} %bitcast.19.core_ref, bf16[1024,2560]{1,0:T(8,128)(2,1)} %rows_ref.1, bf16[1024,1920]{1,0:T(8,128)(2,1)S(1)} %copy-done.30), custom_call_target="tpu_custom_call" | custom-call | flops 10066329600 | bytes 19005440 | tf_op jit(solution)/shard_map/pair_grad/pallas_call | solution.py:325
  495.0 9.9 %collective-permute-done.16 = bf16[2,512,640]{2,1,0:T(8,128)(2,1)S(1)} collective-permute-done((bf16[2,512,640]{2,1,0:T(8,128)(2,1)}, bf16[2,512,640]{2,1,0:T(8,128)(2,1)S(1)}, u32[]{:S(2)}, u32[]{:S(2)}) %collective-permute-start.16) | collective-permute-done | bytes 1310752 | tf_op jit(solution)/shard_map/ppermute | solution.py:38
  508.6 12.4 %collective-permute-done.21 = f32[8,128]{1,0:T(8,128)S(1)} collective-permute-done((f32[8,128]{1,0:T(8,128)S(1)}, f32[8,128]{1,0:T(8,128)S(1)}, u32[]{:S(2)}, u32[]{:S(2)}) %collective-permute-start.21) | collective-permute-done | bytes 4128 | tf_op jit(solution)/shard_map/ppermute | solution.py:38
  523.3 4.0 fusion.54
  530.1 26.3 %collective-permute-done.26.along_x = bf16[1024,640]{1,0:T(8,128)(2,1)S(1)} collective-permute-done((bf16[1024,640]{1,0:T(8,128)(2,1)S(1)}, bf16[1024,640]{1,0:T(8,128)(2,1)S(1)}, u32[]{:S(2)}, u32[]{:S(2)}) %collective-permute-start.26) | collective-permute-done | bytes 1310752 | tf_op jit(solution)/shard_map/ppermute | solution.py:38
  559.6 12.0 %collective-permute-done.28.top = bf16[512,640]{1,0:T(8,128)(2,1)S(1)} collective-permute-done((bf16[512,640]{1,0:T(8,128)(2,1)S(1)}, bf16[512,640]{1,0:T(8,128)(2,1)S(1)}, u32[]{:S(2)}, u32[]{:S(2)}) %collective-permute-start.28) | collective-permute-done | bytes 655392 | tf_op jit(solution)/shard_map/ppermute | solution.py:38
  572.2 5.4 pieces_product.1
  578.7 4.3 all-to-all-start.2
  583.1 13.9 %all-to-all-done.2 = bf16[4,256,640]{2,1,0:T(8,128)(2,1)} async-done(((bf16[4,256,640]{2,1,0:T(8,128)(2,1)}), bf16[4,256,640]{2,1,0:T(8,128)(2,1)}, u32[]{:S(2)}, u32[]{:S(2)}) %all-to-all-start.2) | async-done | bytes 1310752 | tf_op jit(solution)/shard_map/all_to_all | solution.py:158
  597.0 2.5 copy.41
  599.5 7.3 add_convert_fusion
  615.7 15.7 %attention_backward.1 = (bf16[256,2560]{1,0:T(8,128)(2,1)S(1)}, f32[1024,512]{1,0:T(8,128)S(1)}) custom-call(s32[1]{0:T(128)} %bitcast.1.first_ref, bf16[256,3072]{1,0:T(8,128)(2,1)S(1)} %bitcast.116, bf16[1024,512]{1,0:T(8,128)(2,1)S(1)} %copy-done.18, f32[256,128]{1,0:T(8,128)S(1)} %copy-done.24, f32[256,128]{1,0:T(8,128)S(1)} %copy-done.22, ...), custom_call_target="tpu_custom_call" | custom-call | flops 6710886400 | bytes 8388608 | tf_op jit(solution)/shard_map/attention_backward/pallas_call | solution.py:260
  634.4 4.6 collective-permute-done.30
  641.2 3.8 collective-permute-done.31
  647.5 4.7 collective-permute-done.33
  656.5 4.4 all-to-all-start.3
  661.3 2.6 broadcast.71
  669.6 7.5 all-to-all-done.3
  678.9 12.1 %attn_grad.1 = (bf16[1280,1408]{1,0:T(8,128)(2,1)S(1)}, bf16[1280,1408]{1,0:T(8,128)(2,1)S(1)}, f32[2560,1]{1,0:T(8,128)S(1)}) custom-call(s32[1]{0:T(128)} %bitcast.19.core_ref, bf16[1024,2560]{1,0:T(8,128)(2,1)} %copy-done.43, bf16[1024,768]{1,0:T(8,128)(2,1)S(1)} %multiply_convert_fusion.1.d_qkv_ref, ...), custom_call_target="tpu_custom_call" | custom-call | flops 7381975040 | bytes 27787264 | tf_op jit(solution)/shard_map/attn_grad/pallas_call | solution.py:477
  691.1 6.3 collective-permute-done.45
  697.4 2.7 add_convert_fusion.3
  700.1 17.0 %scatter_product.6 = (bf16[2,512,640]{2,1,0:T(8,128)(2,1)S(1)}, bf16[2,512,640]{2,1,0:T(8,128)(2,1)S(1)}, bf16[2,512,640]{2,1,0:T(8,128)(2,1)S(1)}, bf16[2,512,640]{2,1,0:T(8,128)(2,1)S(1)}) custom-call(s32[1]{0:T(128)} %bitcast.me_ref, bf16[1024,1920]{1,0:T(8,128)(2,1)} %get-tuple-element.69.refs_0_.right_ref, ...), custom_call_target="tpu_custom_call" | custom-call | flops 10066329600 | bytes 19005440 | tf_op jit(solution)/shard_map/scatter_product/pallas_call | solution.py:376
  719.1 28.9 %collective-permute-done.22 = bf16[2,512,640]{2,1,0:T(8,128)(2,1)S(1)} collective-permute-done((bf16[2,512,640]{2,1,0:T(8,128)(2,1)S(1)}, bf16[2,512,640]{2,1,0:T(8,128)(2,1)S(1)}, u32[]{:S(2)}, u32[]{:S(2)}) %collective-permute-start.22) | collective-permute-done | bytes 1310752 | tf_op jit(solution)/shard_map/ppermute | solution.py:38
  750.7 9.3 %scatter_product.7 = (bf16[2,512,640]{2,1,0:T(8,128)(2,1)}, bf16[2,512,640]{2,1,0:T(8,128)(2,1)S(1)}, bf16[2,512,640]{2,1,0:T(8,128)(2,1)S(1)}, bf16[2,512,640]{2,1,0:T(8,128)(2,1)S(1)}) custom-call(s32[1]{0:T(128)} %bitcast.me_ref, bf16[1024,768]{1,0:T(8,128)(2,1)} %bitcast.35.refs_0_, bf16[2560,1408]{1,0:T(8,128)(2,1)} %all-gather.4.cloned.1.call-done.refs_1_.weight_ref), custom_call_target="tpu_custom_call" | custom-call | flops 4026531840 | bytes 14024704 | tf_op jit(solution)/shard_map/scatter_product/pallas_call | solution.py:376
  766.9 2.8 bitcast_add_fusion.3
  769.7 35.7 %collective-permute-done.40 = f32[8,320]{1,0:T(8,128)S(1)} collective-permute-done((f32[8,320]{1,0:T(8,128)S(1)}, f32[8,320]{1,0:T(8,128)S(1)}, u32[]{:S(2)}, u32[]{:S(2)}) %collective-permute-start.40) | collective-permute-done | bytes 10272 | tf_op jit(solution)/shard_map/ppermute | solution.py:38
  809.1 2.6 bitcast_add_fusion.2
  812.7 2.8 collective-permute-done.43
  823.0 11.1 %collective-permute-done.35 = bf16[512,640]{1,0:T(8,128)(2,1)S(1)} collective-permute-done((bf16[512,640]{1,0:T(8,128)(2,1)}, bf16[512,640]{1,0:T(8,128)(2,1)S(1)}, u32[]{:S(2)}, u32[]{:S(2)}) %collective-permute-start.35) | collective-permute-done | bytes 655392 | tf_op jit(solution)/shard_map/ppermute | solution.py:38
  836.6 2.6 bitcast_add_fusion
  839.2 6.1 convert_multiply_fusion.3
  846.7 4.7 fusion.12
  852.1 2.9 convert_bitcast_fusion
  (340 shorter events, 130.4 us)
Async XLA Ops:
  7.2 79.2 %all-gather.4.cloned.1.call-start = ((), (), s32[]{:S(2)}) async-start(), calls=%async_computation.8 | async-start | bytes 8110080 | tf_op jit(solution)/shard_map/all_gather | solution.py:546
  11.3 265.7 %all-gather.6.cloned.1.call-start = ((), (), s32[]{:S(2)}) async-start(), calls=%async_computation.9 | async-start | bytes 22118400 | tf_op jit(solution)/shard_map/all_gather | solution.py:546
  13.6 342.2 %all-gather.8.cloned.1.call-start = ((), (), s32[]{:S(2)}) async-start(), calls=%async_computation.10 | async-start | bytes 11059200 | tf_op jit(solution)/shard_map/all_gather | solution.py:546
  13.8 31.7 %collective-permute-start = (bf16[1024,640]{1,0:T(8,128)(2,1)S(1)}, bf16[1024,640]{1,0:T(8,128)(2,1)S(1)}, u32[]{:S(2)}, u32[]{:S(2)}) collective-permute-start(bf16[1024,640]{1,0:T(8,128)(2,1)S(1)} %copy-done.39), channel_id=1, source_target_pairs={{0,1},{1,0},{2,3},{3,2},{4,5},{5,4},{6,7},{7,6},{8,9},{9,8},{10,11... | collective-permute-start | bytes 3932168 | tf_op jit(solution)/shard_map/ppermute | solution.py:38
  16.8 31.4 %collective-permute-start.1 = (bf16[1024,640]{1,0:T(8,128)(2,1)S(1)}, bf16[1024,640]{1,0:T(8,128)(2,1)S(1)}, u32[]{:S(2)}, u32[]{:S(2)}) collective-permute-start(bf16[1024,640]{1,0:T(8,128)(2,1)S(1)} %copy-done.39), channel_id=1, source_target_pairs={{0,2},{1,3},{2,0},{3,1},{4,6},{5,7},{6,4},{7,5},{8,10},{9,11},{10,... | collective-permute-start | bytes 3932168 | tf_op jit(solution)/shard_map/ppermute | solution.py:38
  46.4 16.2 %collective-permute-start.2 = (bf16[512,640]{1,0:T(8,128)(2,1)}, bf16[512,640]{1,0:T(8,128)(2,1)S(1)}, u32[]{:S(2)}, u32[]{:S(2)}) collective-permute-start(bf16[512,640]{1,0:T(8,128)(2,1)} %slice.228), channel_id=1, source_target_pairs={{0,2},{1,3},{2,0},{3,1},{4,6},{5,7},{6,4},{7,5},{8,10},{9,11},{10,... | collective-permute-start | bytes 1966088 | tf_op jit(solution)/shard_map/ppermute | solution.py:38
  50.2 15.8 %collective-permute-start.3 = (bf16[512,640]{1,0:T(8,128)(2,1)}, bf16[512,640]{1,0:T(8,128)(2,1)}, u32[]{:S(2)}, u32[]{:S(2)}) collective-permute-start(bf16[512,640]{1,0:T(8,128)(2,1)} %slice.229), channel_id=1, source_target_pairs={{0,1},{1,0},{2,3},{3,2},{4,5},{5,4},{6,7},{7,6},{8,9},{9,8},{10,11... | collective-permute-start | bytes 1966088 | tf_op jit(solution)/shard_map/ppermute | solution.py:38
  95.5 23.6 %all-to-all-start = ((bf16[4,256,768]{2,1,0:T(8,128)(2,1)}), bf16[4,256,768]{2,1,0:T(8,128)(2,1)S(1)}, u32[]{:S(2)}, u32[]{:S(2)}) async-start(bf16[4,256,768]{2,1,0:T(8,128)(2,1)} %bitcast.3), calls=%async_computation | async-start | bytes 3145728 | tf_op jit(solution)/shard_map/all_to_all | solution.py:158
  99.3 739.8 %reduce-scatter.7.cloned.1.call-start = ((), (), s32[]{:S(2)}) async-start(), calls=%async_computation.12 | async-start | bytes 6144000 | tf_op jit(solution)/shard_map/reduce_scatter | solution.py:554
  121.7 7.8 collective-permute-start.4
  123.1 8.0 collective-permute-start.5
  129.6 5.0 collective-permute-start.6
  131.1 5.0 collective-permute-start.7
  173.5 27.2 %collective-permute-start.8 = (bf16[2,512,640]{2,1,0:T(8,128)(2,1)S(1)}, bf16[2,512,640]{2,1,0:T(8,128)(2,1)S(1)}, u32[]{:S(2)}, u32[]{:S(2)}) collective-permute-start(bf16[2,512,640]{2,1,0:T(8,128)(2,1)S(1)} %get-tuple-element.56), channel_id=1, source_target_pairs={{0,1},{1,0},{2,3},{3,2},{4,5},{5,4},{6,7},{7,6},{8,9},{9,8},{10,11... | collective-permute-start | bytes 3932168 | tf_op jit(solution)/shard_map/ppermute | solution.py:38
  174.6 29.6 %collective-permute-start.10 = (bf16[2,512,640]{2,1,0:T(8,128)(2,1)S(1)}, bf16[2,512,640]{2,1,0:T(8,128)(2,1)S(1)}, u32[]{:S(2)}, u32[]{:S(2)}) collective-permute-start(bf16[2,512,640]{2,1,0:T(8,128)(2,1)S(1)} %get-tuple-element.58), channel_id=1, source_target_pairs={{0,2},{1,3},{2,0},{3,1},{4,6},{5,7},{6,4},{7,5},{8,10},{9,11},{10,... | collective-permute-start | bytes 3932168 | tf_op jit(solution)/shard_map/ppermute | solution.py:38
  200.9 14.9 %collective-permute-start.9 = (bf16[512,640]{1,0:T(8,128)(2,1)S(1)}, bf16[512,640]{1,0:T(8,128)(2,1)S(1)}, u32[]{:S(2)}, u32[]{:S(2)}) collective-permute-start(bf16[512,640]{1,0:T(8,128)(2,1)S(1)} %fusion.20), channel_id=1, source_target_pairs={{0,2},{1,3},{2,0},{3,1},{4,6},{5,7},{6,4},{7,5},{8,10},{9,11},{10,... | collective-permute-start | bytes 1966088 | tf_op jit(solution)/shard_map/ppermute | solution.py:38
  204.3 11.6 %collective-permute-start.11 = (bf16[512,640]{1,0:T(8,128)(2,1)S(1)}, bf16[512,640]{1,0:T(8,128)(2,1)S(1)}, u32[]{:S(2)}, u32[]{:S(2)}) collective-permute-start(bf16[512,640]{1,0:T(8,128)(2,1)S(1)} %fusion.21), channel_id=1, source_target_pairs={{0,1},{1,0},{2,3},{3,2},{4,5},{5,4},{6,7},{7,6},{8,9},{9,8},{10,11... | collective-permute-start | bytes 1966088 | tf_op jit(solution)/shard_map/ppermute | solution.py:38
  220.6 28.0 %collective-permute-start.12 = (bf16[1024,640]{1,0:T(8,128)(2,1)S(1)}, bf16[1024,640]{1,0:T(8,128)(2,1)S(1)}, u32[]{:S(2)}, u32[]{:S(2)}) collective-permute-start(bf16[1024,640]{1,0:T(8,128)(2,1)S(1)} %get-tuple-element.102), channel_id=1, source_target_pairs={{0,1},{1,0},{2,3},{3,2},{4,5},{5,4},{6,7},{7,6},{8,9},{9,8},{10,11... | collective-permute-start | bytes 3932168 | tf_op jit(solution)/shard_map/ppermute | solution.py:38
  221.4 28.7 %collective-permute-start.13 = (bf16[1024,640]{1,0:T(8,128)(2,1)S(1)}, bf16[1024,640]{1,0:T(8,128)(2,1)S(1)}, u32[]{:S(2)}, u32[]{:S(2)}) collective-permute-start(bf16[1024,640]{1,0:T(8,128)(2,1)S(1)} %get-tuple-element.102), channel_id=1, source_target_pairs={{0,2},{1,3},{2,0},{3,1},{4,6},{5,7},{6,4},{7,5},{8,10},{9,11},{10,... | collective-permute-start | bytes 3932168 | tf_op jit(solution)/shard_map/ppermute | solution.py:38
  249.6 13.5 %collective-permute-start.14 = (bf16[512,640]{1,0:T(8,128)(2,1)}, bf16[512,640]{1,0:T(8,128)(2,1)S(1)}, u32[]{:S(2)}, u32[]{:S(2)}) collective-permute-start(bf16[512,640]{1,0:T(8,128)(2,1)} %slice.241), channel_id=1, source_target_pairs={{0,2},{1,3},{2,0},{3,1},{4,6},{5,7},{6,4},{7,5},{8,10},{9,11},{10,... | collective-permute-start | bytes 1966088 | tf_op jit(solution)/shard_map/ppermute | solution.py:38
  250.9 13.5 %collective-permute-start.15 = (bf16[512,640]{1,0:T(8,128)(2,1)}, bf16[512,640]{1,0:T(8,128)(2,1)}, u32[]{:S(2)}, u32[]{:S(2)}) collective-permute-start(bf16[512,640]{1,0:T(8,128)(2,1)} %slice.242), channel_id=1, source_target_pairs={{0,1},{1,0},{2,3},{3,2},{4,5},{5,4},{6,7},{7,6},{8,9},{9,8},{10,11... | collective-permute-start | bytes 1966088 | tf_op jit(solution)/shard_map/ppermute | solution.py:38
  395.1 8.5 collective-permute-start.46
  409.5 429.6 %reduce-scatter.9.cloned.1.call-start = ((), (), s32[]{:S(2)}) async-start(), calls=%async_computation.13 | async-start | bytes 6144000 | tf_op jit(solution)/shard_map/reduce_scatter | solution.py:554
  459.4 8.4 collective-permute-start.47
  473.8 31.1 %collective-permute-start.16 = (bf16[2,512,640]{2,1,0:T(8,128)(2,1)}, bf16[2,512,640]{2,1,0:T(8,128)(2,1)S(1)}, u32[]{:S(2)}, u32[]{:S(2)}) collective-permute-start(bf16[2,512,640]{2,1,0:T(8,128)(2,1)} %copy-done.27), channel_id=1, source_target_pairs={{0,1},{1,0},{2,3},{3,2},{4,5},{5,4},{6,7},{7,6},{8,9},{9,8},{10,11... | collective-permute-start | bytes 3932168 | tf_op jit(solution)/shard_map/ppermute | solution.py:38
  475.0 31.3 %collective-permute-start.18 = (bf16[2,512,640]{2,1,0:T(8,128)(2,1)}, bf16[2,512,640]{2,1,0:T(8,128)(2,1)S(1)}, u32[]{:S(2)}, u32[]{:S(2)}) collective-permute-start(bf16[2,512,640]{2,1,0:T(8,128)(2,1)} %copy-done.26), channel_id=1, source_target_pairs={{0,2},{1,3},{2,0},{3,1},{4,6},{5,7},{6,4},{7,5},{8,10},{9,11},{10,... | collective-permute-start | bytes 3932168 | tf_op jit(solution)/shard_map/ppermute | solution.py:38
  494.3 105.2 %collective-permute-start.50 = (bf16[1280,1920]{1,0:T(8,128)(2,1)}, bf16[1280,1920]{1,0:T(8,128)(2,1)}, u32[]{:S(2)}, u32[]{:S(2)}) collective-permute-start(bf16[1280,1920]{1,0:T(8,128)(2,1)} %get-tuple-element.98), channel_id=1, source_target_pairs={{0,4},{4,0},{8,12},{12,8},{16,20},{20,16},{24,28},{28,24},{1,5},{5... | collective-permute-start | bytes 14745608 | tf_op jit(solution)/shard_map/ppermute | solution.py:551
  494.4 13.7 %collective-permute-start.20 = (f32[8,128]{1,0:T(8,128)S(1)}, f32[8,128]{1,0:T(8,128)S(1)}, u32[]{:S(2)}, u32[]{:S(2)}) collective-permute-start(f32[8,128]{1,0:T(8,128)S(1)} %bitcast.129), channel_id=1, source_target_pairs={{0,1},{1,0},{2,3},{3,2},{4,5},{5,4},{6,7},{7,6},{8,9},{9,8},{10,11... | collective-permute-start | bytes 12296 | tf_op jit(solution)/shard_map/ppermute | solution.py:38
  505.0 16.0 %collective-permute-start.17 = (bf16[512,640]{1,0:T(8,128)(2,1)S(1)}, bf16[512,640]{1,0:T(8,128)(2,1)S(1)}, u32[]{:S(2)}, u32[]{:S(2)}) collective-permute-start(bf16[512,640]{1,0:T(8,128)(2,1)S(1)} %fusion.22), channel_id=1, source_target_pairs={{0,2},{1,3},{2,0},{3,1},{4,6},{5,7},{6,4},{7,5},{8,10},{9,11},{10,... | collective-permute-start | bytes 1966088 | tf_op jit(solution)/shard_map/ppermute | solution.py:38
  506.5 15.7 %collective-permute-start.19 = (bf16[512,640]{1,0:T(8,128)(2,1)S(1)}, bf16[512,640]{1,0:T(8,128)(2,1)S(1)}, u32[]{:S(2)}, u32[]{:S(2)}) collective-permute-start(bf16[512,640]{1,0:T(8,128)(2,1)S(1)} %fusion.23), channel_id=1, source_target_pairs={{0,1},{1,0},{2,3},{3,2},{4,5},{5,4},{6,7},{7,6},{8,9},{9,8},{10,11... | collective-permute-start | bytes 1966088 | tf_op jit(solution)/shard_map/ppermute | solution.py:38
  508.1 13.0 %collective-permute-start.21 = (f32[8,128]{1,0:T(8,128)S(1)}, f32[8,128]{1,0:T(8,128)S(1)}, u32[]{:S(2)}, u32[]{:S(2)}) collective-permute-start(f32[8,128]{1,0:T(8,128)S(1)} %bitcast_add_fusion.8), channel_id=1, source_target_pairs={{0,2},{1,3},{2,0},{3,1},{4,6},{5,7},{6,4},{7,5},{8,10},{9,11},{10,... | collective-permute-start | bytes 12296 | tf_op jit(solution)/shard_map/ppermute | solution.py:38
  522.2 50.0 %slice-start = ((s8[7208960]{0:T(1024)(128)(4,1)}), s8[4194304]{0:T(1024)(128)(4,1)S(1)}, s32[]{:S(2)}) async-start(s8[7208960]{0:T(1024)(128)(4,1)} %bitcast.111), calls=%async_computation.15 | async-start | bytes 8388608
  523.3 48.9 %slice-start.1 = ((s8[7208960]{0:T(1024)(128)(4,1)}), s8[3014656]{0:T(1024)(128)(4,1)S(1)}, s32[]{:S(2)}) async-start(s8[7208960]{0:T(1024)(128)(4,1)} %bitcast.111), calls=%async_computation.16 | async-start | bytes 6029312
  527.3 29.1 %collective-permute-start.26 = (bf16[1024,640]{1,0:T(8,128)(2,1)S(1)}, bf16[1024,640]{1,0:T(8,128)(2,1)S(1)}, u32[]{:S(2)}, u32[]{:S(2)}) collective-permute-start(bf16[1024,640]{1,0:T(8,128)(2,1)S(1)} %get-tuple-element.77.own), channel_id=1, source_target_pairs={{0,1},{1,0},{2,3},{3,2},{4,5},{5,4},{6,7},{7,6},{8,9},{9,8},{10,11... | collective-permute-start | bytes 3932168 | tf_op jit(solution)/shard_map/ppermute | solution.py:38
  528.7 29.6 %collective-permute-start.27 = (bf16[1024,640]{1,0:T(8,128)(2,1)S(1)}, bf16[1024,640]{1,0:T(8,128)(2,1)S(1)}, u32[]{:S(2)}, u32[]{:S(2)}) collective-permute-start(bf16[1024,640]{1,0:T(8,128)(2,1)S(1)} %get-tuple-element.77.own), channel_id=1, source_target_pairs={{0,2},{1,3},{2,0},{3,1},{4,6},{5,7},{6,4},{7,5},{8,10},{9,11},{10,... | collective-permute-start | bytes 3932168 | tf_op jit(solution)/shard_map/ppermute | solution.py:38
  556.5 15.1 %collective-permute-start.28 = (bf16[512,640]{1,0:T(8,128)(2,1)S(1)}, bf16[512,640]{1,0:T(8,128)(2,1)S(1)}, u32[]{:S(2)}, u32[]{:S(2)}) collective-permute-start(bf16[512,640]{1,0:T(8,128)(2,1)S(1)} %slice.253), channel_id=1, source_target_pairs={{0,2},{1,3},{2,0},{3,1},{4,6},{5,7},{6,4},{7,5},{8,10},{9,11},{10,... | collective-permute-start | bytes 1966088 | tf_op jit(solution)/shard_map/ppermute | solution.py:38
  558.3 13.9 %collective-permute-start.29 = (bf16[512,640]{1,0:T(8,128)(2,1)S(1)}, bf16[512,640]{1,0:T(8,128)(2,1)S(1)}, u32[]{:S(2)}, u32[]{:S(2)}) collective-permute-start(bf16[512,640]{1,0:T(8,128)(2,1)S(1)} %slice.254), channel_id=1, source_target_pairs={{0,1},{1,0},{2,3},{3,2},{4,5},{5,4},{6,7},{7,6},{8,9},{9,8},{10,11... | collective-permute-start | bytes 1966088 | tf_op jit(solution)/shard_map/ppermute | solution.py:38
  578.7 18.3 %all-to-all-start.2 = ((bf16[4,256,640]{2,1,0:T(8,128)(2,1)}), bf16[4,256,640]{2,1,0:T(8,128)(2,1)}, u32[]{:S(2)}, u32[]{:S(2)}) async-start(bf16[4,256,640]{2,1,0:T(8,128)(2,1)} %bitcast.113), calls=%async_computation.2 | async-start | bytes 2621440 | tf_op jit(solution)/shard_map/all_to_all | solution.py:158
  583.0 269.0 %reduce-scatter.11.cloned.1.call-start = ((), (), s32[]{:S(2)}) async-start(), calls=%async_computation.14 | async-start | bytes 6144000 | tf_op jit(solution)/shard_map/reduce_scatter | solution.py:554
  631.7 7.3 collective-permute-start.30
  633.9 6.6 collective-permute-start.32
  639.7 5.3 collective-permute-start.31
  646.9 5.3 collective-permute-start.33
  656.5 20.7 %all-to-all-start.3 = ((bf16[256,4,768]{2,0,1:T(8,128)(2,1)}), bf16[256,4,768]{2,0,1:T(8,128)(2,1)}, u32[]{:S(2)}, u32[]{:S(2)}) async-start(bf16[256,4,768]{2,0,1:T(8,128)(2,1)} %bitcast.124), calls=%async_computation.3 | async-start | bytes 3145728 | tf_op jit(solution)/shard_map/all_to_all | solution.py:162
  660.9 194.8 %reduce-scatter.5.cloned.1.call-start = ((), (), s32[]{:S(2)}) async-start(), calls=%async_computation.11 | async-start | bytes 4505600 | tf_op jit(solution)/shard_map/reduce_scatter | solution.py:554
  691.1 6.4 collective-permute-start.45
  717.2 44.4 %copy-start.15 = (bf16[2,512,640]{2,1,0:T(8,128)(2,1)}, bf16[2,512,640]{2,1,0:T(8,128)(2,1)S(1)}, u32[]{:S(2)}) copy-start(bf16[2,512,640]{2,1,0:T(8,128)(2,1)S(1)} %get-tuple-element.72) | copy-start | bytes 3932164
  717.2 30.9 %collective-permute-start.22 = (bf16[2,512,640]{2,1,0:T(8,128)(2,1)S(1)}, bf16[2,512,640]{2,1,0:T(8,128)(2,1)S(1)}, u32[]{:S(2)}, u32[]{:S(2)}) collective-permute-start(bf16[2,512,640]{2,1,0:T(8,128)(2,1)S(1)} %get-tuple-element.71), channel_id=1, source_target_pairs={{0,1},{1,0},{2,3},{3,2},{4,5},{5,4},{6,7},{7,6},{8,9},{9,8},{10,11... | collective-permute-start | bytes 3932168 | tf_op jit(solution)/shard_map/ppermute | solution.py:38
  718.7 42.9 %collective-permute-start.24 = (bf16[2,512,640]{2,1,0:T(8,128)(2,1)S(1)}, bf16[2,512,640]{2,1,0:T(8,128)(2,1)S(1)}, u32[]{:S(2)}, u32[]{:S(2)}) collective-permute-start(bf16[2,512,640]{2,1,0:T(8,128)(2,1)S(1)} %get-tuple-element.73), channel_id=1, source_target_pairs={{0,2},{1,3},{2,0},{3,1},{4,6},{5,7},{6,4},{7,5},{8,10},{9,11},{10,... | collective-permute-start | bytes 3932168 | tf_op jit(solution)/shard_map/ppermute | solution.py:38
  749.2 17.8 %collective-permute-start.23 = (bf16[512,640]{1,0:T(8,128)(2,1)}, bf16[512,640]{1,0:T(8,128)(2,1)}, u32[]{:S(2)}, u32[]{:S(2)}) collective-permute-start(bf16[512,640]{1,0:T(8,128)(2,1)} %fusion.24), channel_id=1, source_target_pairs={{0,2},{1,3},{2,0},{3,1},{4,6},{5,7},{6,4},{7,5},{8,10},{9,11},{10,... | collective-permute-start | bytes 1966088 | tf_op jit(solution)/shard_map/ppermute | solution.py:38
  761.1 55.1 %collective-permute-start.34 = (bf16[2,512,640]{2,1,0:T(8,128)(2,1)}, bf16[2,512,640]{2,1,0:T(8,128)(2,1)}, u32[]{:S(2)}, u32[]{:S(2)}) collective-permute-start(bf16[2,512,640]{2,1,0:T(8,128)(2,1)} %get-tuple-element.85), channel_id=1, source_target_pairs={{0,1},{1,0},{2,3},{3,2},{4,5},{5,4},{6,7},{7,6},{8,9},{9,8},{10,11... | collective-permute-start | bytes 3932168 | tf_op jit(solution)/shard_map/ppermute | solution.py:38
  762.8 46.3 %collective-permute-start.25 = (bf16[512,640]{1,0:T(8,128)(2,1)}, bf16[512,640]{1,0:T(8,128)(2,1)S(1)}, u32[]{:S(2)}, u32[]{:S(2)}) collective-permute-start(bf16[512,640]{1,0:T(8,128)(2,1)} %fusion.25), channel_id=1, source_target_pairs={{0,1},{1,0},{2,3},{3,2},{4,5},{5,4},{6,7},{7,6},{8,9},{9,8},{10,11... | collective-permute-start | bytes 1966088 | tf_op jit(solution)/shard_map/ppermute | solution.py:38
  764.9 40.5 %collective-permute-start.40 = (f32[8,320]{1,0:T(8,128)S(1)}, f32[8,320]{1,0:T(8,128)S(1)}, u32[]{:S(2)}, u32[]{:S(2)}) collective-permute-start(f32[8,320]{1,0:T(8,128)S(1)} %reshape.170), channel_id=1, source_target_pairs={{0,1},{1,0},{2,3},{3,2},{4,5},{5,4},{6,7},{7,6},{8,9},{9,8},{10,11... | collective-permute-start | bytes 30728 | tf_op jit(solution)/shard_map/ppermute | solution.py:38
  765.4 53.3 %collective-permute-start.36 = (bf16[2,512,640]{2,1,0:T(8,128)(2,1)}, bf16[2,512,640]{2,1,0:T(8,128)(2,1)}, u32[]{:S(2)}, u32[]{:S(2)}) collective-permute-start(bf16[2,512,640]{2,1,0:T(8,128)(2,1)} %copy-done.25), channel_id=1, source_target_pairs={{0,2},{1,3},{2,0},{3,1},{4,6},{5,7},{6,4},{7,5},{8,10},{9,11},{10,... | collective-permute-start | bytes 3932168 | tf_op jit(solution)/shard_map/ppermute | solution.py:38
  805.4 3.7 collective-permute-start.41
  806.5 5.3 collective-permute-start.38
  809.1 2.6 collective-permute-start.42
  811.7 3.8 collective-permute-start.43
  812.0 10.2 %collective-permute-start.39 = (f32[4,256]{1,0:T(4,128)S(1)}, f32[4,256]{1,0:T(4,128)S(1)}, u32[]{:S(2)}, u32[]{:S(2)}) collective-permute-start(f32[4,256]{1,0:T(4,128)S(1)} %add.393), channel_id=1, source_target_pairs={{0,2},{1,3},{2,0},{3,1},{4,6},{5,7},{6,4},{7,5},{8,10},{9,11},{10,... | collective-permute-start | bytes 12296 | tf_op jit(solution)/shard_map/ppermute | solution.py:38
  815.5 6.8 collective-permute-start.44
  818.2 15.9 %collective-permute-start.35 = (bf16[512,640]{1,0:T(8,128)(2,1)}, bf16[512,640]{1,0:T(8,128)(2,1)S(1)}, u32[]{:S(2)}, u32[]{:S(2)}) collective-permute-start(bf16[512,640]{1,0:T(8,128)(2,1)} %fusion.26), channel_id=1, source_target_pairs={{0,2},{1,3},{2,0},{3,1},{4,6},{5,7},{6,4},{7,5},{8,10},{9,11},{10,... | collective-permute-start | bytes 1966088 | tf_op jit(solution)/shard_map/ppermute | solution.py:38
  820.8 15.7 %collective-permute-start.37 = (bf16[512,640]{1,0:T(8,128)(2,1)}, bf16[512,640]{1,0:T(8,128)(2,1)}, u32[]{:S(2)}, u32[]{:S(2)}) collective-permute-start(bf16[512,640]{1,0:T(8,128)(2,1)} %fusion.27), channel_id=1, source_target_pairs={{0,1},{1,0},{2,3},{3,2},{4,5},{5,4},{6,7},{7,6},{8,9},{9,8},{10,11... | collective-permute-start | bytes 1966088 | tf_op jit(solution)/shard_map/ppermute | solution.py:38
  845.2 6.1 collective-permute-start.48
  851.4 3.7 collective-permute-start.49
  (70 other events, 650.8 us)
Sparse Core Ops, SparseCore 0:
  11.4 74.9 all-gather.3
  88.7 173.2 all-gather.5
  263.6 92.1 all-gather.7
  409.6 86.8 reduce-scatter.6
  498.7 88.9 reduce-scatter.8
  607.0 86.0 reduce-scatter.10
  700.2 65.0 reduce-scatter.4

commit v4 on v3

--- a/solution.py
+++ b/solution.py
@@ -108,22 +108,6 @@
     return block, along_x, along_y, top, bottom
 
 
-def assemble(pieces):
-    me = lax.axis_index("mdl")
-    own, along_x, along_y, top, bottom = pieces
-    rows, width = own.shape
-    whole = jnp.zeros((rows, 4 * width), own.dtype)
-    for piece, source, row in (
-        (own, me, 0),
-        (along_x, me ^ 1, 0),
-        (along_y, me ^ 2, 0),
-        (top, me ^ 3, 0),
-        (bottom, me ^ 3, rows // 2),
-    ):
-        whole = lax.dynamic_update_slice(whole, piece, (row, source * width))
-    return whole
-
-
 def scatter_payload(payload):
     top_sent, bottom_sent, top_kept, bottom_kept = payload
     got_top = swap(top_sent, 1)
@@ -160,6 +144,18 @@
 
 def cols_to_rows(block):
     return lax.all_to_all(block, "mdl", split_axis=1, concat_axis=0, tiled=True)
+
+
+def in_order(mebibytes):
+    return pltpu.CompilerParams(
+        dimension_semantics=(pltpu.ARBITRARY,), vmem_limit_bytes=mebibytes << 20
+    )
+
+
+def cost(flops, bytes_accessed, transcendentals=0):
+    return pl.CostEstimate(
+        flops=flops, bytes_accessed=bytes_accessed, transcendentals=transcendentals
+    )
 
 
 def turn(vector, cos, sin):
@@ -242,14 +238,8 @@
             whole_spec((rows, 1)),
         ],
         out_specs=(head_spec, pl.BlockSpec((1, rows, 1), lambda head: (head, 0, 0))),
-        compiler_params=pltpu.CompilerParams(
-            dimension_semantics=("arbitrary",), vmem_limit_bytes=32 << 20
-        ),
-        cost_estimate=pl.CostEstimate(
-            flops=4 * rows * keys * HEADS * HEAD,
-            bytes_accessed=4 * rows * HEADS * HEAD + 4 * keys * HEAD,
-            transcendentals=rows * keys * HEADS,
-        ),
+        compiler_params=in_order(32),
+        cost_estimate=cost(4 * rows * keys * HEADS * HEAD, 4 * rows * HEADS * HEAD + 4 * keys * HEAD, rows * keys * HEADS),
         name="attention_forward",
     )(first, qkv, kv, cos, sin, pos)
 
@@ -276,31 +266,28 @@
             pl.BlockSpec((1, rows, 1), lambda head: (head, 0, 0)),
         ],
         out_specs=(head_spec, whole_spec((keys, 2 * HEAD))),
-        compiler_params=pltpu.CompilerParams(
-            dimension_semantics=("arbitrary",), vmem_limit_bytes=40 << 20
-        ),
-        cost_estimate=pl.CostEstimate(
-            flops=10 * rows * keys * HEADS * HEAD,
-            bytes_accessed=8 * rows * HEADS * HEAD + 12 * keys * HEAD,
-            transcendentals=rows * keys * HEADS,
-        ),
+        compiler_params=in_order(40),
+        cost_estimate=cost(10 * rows * keys * HEADS * HEAD, 8 * rows * HEADS * HEAD + 12 * keys * HEAD, rows * keys * HEADS),
         name="attention_backward",
     )(first, qkv, kv, cos, sin, pos, att, d_att, norm)
 
 
-def pair_kernel(core_ref, rows_ref, right_ref, kept_ref, sent_ref):
-    total = tn(rows_ref[...], right_ref[...]).astype(BF16)
+def keep_half(core_ref, total, kept, sent):
     half = total.shape[0] // 2
-
-    @pl.when(core_ref[0] == 0)
-    def _():
-        kept_ref[...] = total[:half]
-        sent_ref[...] = total[half:]
-
-    @pl.when(core_ref[0] == 1)
-    def _():
-        kept_ref[...] = total[half:]
-        sent_ref[...] = total[:half]
+    for core, (first, second) in enumerate(((kept, sent), (sent, kept))):
+
+        @pl.when(core_ref[0] == core)
+        def _(first=first, second=second):
+            first[...] = total[:half]
+            second[...] = total[half:]
+
+
+def pair_kernel(core_ref, left_ref, right_ref, *refs):
+    total = tn(left_ref[...], right_ref[...])
+    if len(refs) == 4:
+        weight = refs[0][:, : total.shape[1]].astype(F32)
+        refs[3][...] = jnp.sum(total * weight, axis=1, keepdims=True)
+    keep_half(core_ref, total.astype(BF16), *refs[-3:-1] if len(refs) == 4 else refs)
 
 
 def split_pairs(total, pairs, core):
@@ -312,36 +299,83 @@
     )
 
 
-def pair_grad(left, right):
+def core_index():
+    return (lax.axis_index("tok") % 2).astype(jnp.int32).reshape(1)
+
+
+def pair_grad(left, right, weight=None):
     tokens, rows = left.shape
     cols = right.shape[1]
     pairs = lax.axis_size("tok") // 2
-    core = lax.axis_index("tok") % 2
     step = rows // pairs
-    if step % 128:
-        return split_pairs(tn(left, right).astype(BF16), pairs, core)
-    out = jax.ShapeDtypeStruct((rows // 2, cols), BF16)
-    out_spec = pl.BlockSpec((step // 2, cols), lambda pair: (pair, 0))
+    if step % 128 or cols % 128:
+        total = tn(left, right)
+        halves = split_pairs(total.astype(BF16), pairs, lax.axis_index("tok") % 2)
+        if weight is None:
+            return halves
+        return *halves, jnp.sum(total * weight[:, :cols].astype(F32), axis=1, keepdims=True)
+    out_shape = [jax.ShapeDtypeStruct((rows // 2, cols), BF16)] * 2
+    out_specs = [pl.BlockSpec((step // 2, cols), lambda pair: (pair, 0))] * 2
+    in_specs = [
+        pl.BlockSpec(memory_space=pltpu.SMEM),
+        pl.BlockSpec((tokens, step), lambda pair: (0, pair)),
+        pl.BlockSpec((tokens, cols), lambda pair: (0, 0)),
+    ]
+    operands = [core_index(), left, right]
+    if weight is not None:
+        operands.append(weight)
+        in_specs.append(pl.BlockSpec((step, weight.shape[1]), lambda pair: (pair, 0)))
+        out_shape.append(jax.ShapeDtypeStruct((rows, 1), F32))
+        out_specs.append(pl.BlockSpec((step, 1), lambda pair: (pair, 0)))
     return pl.pallas_call(
         pair_kernel,
         grid=(pairs,),
+        out_shape=out_shape,
+        in_specs=in_specs,
+        out_specs=out_specs,
+        compiler_params=in_order(48),
+        cost_estimate=cost(2 * tokens * rows * cols, 2 * (tokens * (rows + cols) + rows * cols)),
+    )(*operands)
+
+
+def pieces_grad_kernel(me_ref, core_ref, own, along_x, along_y, top, bottom, right_ref, kept, sent):
+    at = pl.program_id(0)
+    half = top.shape[0]
+    for index, piece in enumerate((own, along_x, along_y)):
+
+        @pl.when(at == index)
+        def _(piece=piece):
+            keep_half(core_ref, tn(piece[...], right_ref[...]).astype(BF16), kept, sent)
+
+    @pl.when(at == 3)
+    def _():
+        total = tn(top[...], right_ref[:half]) + tn(bottom[...], right_ref[half:])
+        keep_half(core_ref, total.astype(BF16), kept, sent)
+
+
+def pieces_grad(pieces, right):
+    tokens, step = pieces[0].shape
+    cols = right.shape[1]
+    me = lax.axis_index("mdl").astype(jnp.int32).reshape(1)
+    out = jax.ShapeDtypeStruct((2 * step, cols), BF16)
+    return pl.pallas_call(
+        pieces_grad_kernel,
+        grid_spec=pltpu.PrefetchScalarGridSpec(
+            num_scalar_prefetch=2,
+            grid=(4,),
+            in_specs=[
+                pl.BlockSpec(array.shape, lambda at, me_ref, core_ref: (0, 0))
+                for array in (*pieces, right)
+            ],
+            out_specs=[
+                pl.BlockSpec((step // 2, cols), lambda at, me_ref, core_ref: (me_ref[0] ^ at, 0))
+            ]
+            * 2,
+        ),
         out_shape=(out, out),
-        in_specs=[
-            pl.BlockSpec(memory_space=pltpu.SMEM),
-            pl.BlockSpec((tokens, step), lambda pair: (0, pair)),
-            pl.BlockSpec((tokens, cols), lambda pair: (0, 0)),
-        ],
-        out_specs=(out_spec, out_spec),
-        compiler_params=pltpu.CompilerParams(
-            dimension_semantics=("arbitrary",), vmem_limit_bytes=48 << 20
-        ),
-        cost_estimate=pl.CostEstimate(
-            flops=2 * tokens * rows * cols,
-            bytes_accessed=2 * (tokens * rows + tokens * cols + rows * cols),
-            transcendentals=0,
-        ),
-        name="pair_grad",
-    )(core.astype(jnp.int32).reshape(1), left, right)
+        compiler_params=in_order(48),
+        cost_estimate=cost(8 * tokens * step * cols, 2 * (4 * tokens * step + 5 * step * cols)),
+    )(me, core_index(), *pieces, right)
 
 
 def payload_kernel(starts, me_ref, *refs):
@@ -383,15 +417,8 @@
             out_specs=[pl.BlockSpec(out.shape, lambda at, me_ref: (0, 0, 0))] * 4,
         ),
         out_shape=(out,) * 4,
-        compiler_params=pltpu.CompilerParams(
-            dimension_semantics=("arbitrary",), vmem_limit_bytes=48 << 20
-        ),
-        cost_estimate=pl.CostEstimate(
-            flops=2 * tokens * rows * depth,
-            bytes_accessed=2 * (tokens * depth + rows * cols + tokens * rows),
-            transcendentals=0,
-        ),
-        name="scatter_product",
+        compiler_params=in_order(48),
+        cost_estimate=cost(2 * tokens * rows * depth, 2 * (tokens * depth + rows * cols + tokens * rows)),
     )(me, *lefts, weight)
 
 
@@ -431,73 +458,9 @@
             scratch_shapes=[pltpu.VMEM((tokens, width), F32)],
         ),
         out_shape=jax.ShapeDtypeStruct((tokens, width), BF16),
-        compiler_params=pltpu.CompilerParams(
-            dimension_semantics=("arbitrary",), vmem_limit_bytes=40 << 20
-        ),
-        cost_estimate=pl.CostEstimate(
-            flops=2 * tokens * rows * width,
-            bytes_accessed=2 * (tokens * rows + rows * cols + tokens * width),
-            transcendentals=0,
-        ),
-        name="pieces_product",
+        compiler_params=in_order(40),
+        cost_estimate=cost(2 * tokens * rows * width, 2 * (tokens * rows + rows * cols + tokens * width)),
     )(me, *pieces, weight)
-
-
-def attn_kernel(core_ref, rows_ref, d_qkv_ref, mixed_ref, heads_ref, weight_ref, kept, sent, gain):
-    cols = d_qkv_ref.shape[1]
-    d_weight = tn(rows_ref[...], d_qkv_ref[...])
-    gain[...] = jnp.sum(d_weight * weight_ref[:, :cols].astype(F32), axis=1, keepdims=True)
-    left = d_weight.astype(BF16)
-    right = tn(mixed_ref[...], heads_ref[...]).astype(BF16)
-    half = left.shape[0] // 2
-    for core, (first, second) in enumerate(((kept, sent), (sent, kept))):
-
-        @pl.when(core_ref[0] == core)
-        def _(first=first, second=second):
-            first[:, :cols] = left[:half]
-            first[:, cols:] = right[:half]
-            second[:, :cols] = left[half:]
-            second[:, cols:] = right[half:]
-
-
-def attn_grad(rows_in, d_qkv, d_mixed, head_block, weight):
-    tokens, rows = rows_in.shape
-    qkv_cols, cols = d_qkv.shape[1], weight.shape[1]
-    pairs = lax.axis_size("tok") // 2
-    core = lax.axis_index("tok") % 2
-    step = rows // pairs
-    if step % 128 or qkv_cols % 128:
-        d_weight = tn(rows_in, d_qkv)
-        gain = jnp.sum(d_weight * weight[:, :qkv_cols].astype(F32), axis=1, keepdims=True)
-        total = jnp.concatenate([d_weight, tn(d_mixed, head_block)], axis=1).astype(BF16)
-        return split_pairs(total, pairs, core), gain
-    out = jax.ShapeDtypeStruct((rows // 2, cols), BF16)
-    out_spec = pl.BlockSpec((step // 2, cols), lambda pair: (pair, 0))
-    left_spec = pl.BlockSpec((tokens, step), lambda pair: (0, pair))
-    kept, sent, gain = pl.pallas_call(
-        attn_kernel,
-        grid=(pairs,),
-        out_shape=(out, out, jax.ShapeDtypeStruct((rows, 1), F32)),
-        in_specs=[
-            pl.BlockSpec(memory_space=pltpu.SMEM),
-            left_spec,
-            pl.BlockSpec(d_qkv.shape, lambda pair: (0, 0)),
-            left_spec,
-            pl.BlockSpec(head_block.shape, lambda pair: (0, 0)),
-            pl.BlockSpec((step, cols), lambda pair: (pair, 0)),
-        ],
-        out_specs=(out_spec, out_spec, pl.BlockSpec((step, 1), lambda pair: (pair, 0))),
-        compiler_params=pltpu.CompilerParams(
-            dimension_semantics=("arbitrary",), vmem_limit_bytes=40 << 20
-        ),
-        cost_estimate=pl.CostEstimate(
-            flops=2 * tokens * rows * cols,
-            bytes_accessed=4 * tokens * rows + 2 * tokens * cols + 4 * rows * cols,
-            transcendentals=0,
-        ),
-        name="attn_grad",
-    )(core.astype(jnp.int32).reshape(1), rows_in, d_qkv, d_mixed, head_block, weight)
-    return (kept, sent), gain
 
 
 def product_to_mdl(lefts, weight, starts):
@@ -615,14 +578,16 @@
     d_mixed_b = after(d_mixed.astype(BF16), up_local[0])
     hidden_later = after(hidden, d_mixed_b)
     ffn_payload, ffn_scatter = product_to_mdl((hidden_later,), w_down_t, (0,))
-    out_cols = head_block.shape[1]
-    if size == 4:
+    if size == 4 and lax.axis_size("tok") == 8:
         pieces = gather_pieces(d_mixed_b)
-        d_head = pieces_product(pieces, w_attn, qkv_cols, out_cols)
-        d_mixed_rows = assemble(tuple(after(piece, d_head) for piece in pieces))
+        d_head = pieces_product(pieces, w_attn, qkv_cols, head_block.shape[1])
+        heads_later = after(head_block, d_head)
+        out_local = pieces_grad(pieces, heads_later)
     else:
         d_mixed_rows = gather_mdl(d_mixed_b, 1)
         d_head = nn(d_mixed_rows, w_attn[:, qkv_cols:]).astype(BF16)
+        out_local = pair_grad(d_mixed_rows, head_block)
+    out_grad = pair_to_tok(out_local).T
     d_attended = rows_to_cols(d_head)
     block_out = (mixed + ffn_scatter(ffn_payload)).astype(BF16)
     d_query, d_kv = attention_backward(
@@ -636,12 +601,10 @@
     stat_rows = jnp.zeros((size, count), F32)
     stat_rows = sum_mdl(lax.dynamic_update_slice(stat_rows, stat_one[None], (me, 0)))
     stat_one = stat_rows.reshape(-1, 1) * (1.0 / features)
-    d_scaled = (d_qkv_part.astype(F32) * scale_one).astype(BF16)
-    attn_local, gain_one = attn_grad(rows_in, d_scaled, d_mixed_rows, head_block, w_attn)
-    attn_sum = pair_to_tok(attn_local)
-    qkv_sum, out_grad = attn_sum[:, :qkv_cols], attn_sum[:, qkv_cols:].T
-    d_later = after(d_qkv_part, attn_local[0])
-    payload, scatter = product_to_mdl((d_later,), w_attn, (0,))
+    payload, scatter = product_to_mdl((d_qkv_part,), w_attn, (0,))
+    d_scaled = (after(d_qkv_part, payload[0]).astype(F32) * scale_one).astype(BF16)
+    *qkv_local, gain_one = pair_grad(rows_in, d_scaled, w_attn)
+    qkv_sum = pair_to_tok(qkv_local)
     d_one = scatter(payload)
     input_grad = d_mixed + scale_one * (d_one - (scale_one * residual) * stat_one)
 
@@ -657,7 +620,7 @@
     )
     gate_grad, up_grad = unfold(gate_sum, norm2_late), unfold(up_sum, norm2_late)
     gain_two_grad = sum_mdl(gain_two)
-    gain_one = sum_tok(sum_mdl(gain_one.reshape(8, -1))).reshape(-1)
+    gain_one = sum_mdl(sum_tok(gain_one.reshape(8, -1))).reshape(-1)
     shard = norm1_gain.shape[0]
     gain_one = lax.dynamic_slice_in_dim(gain_one, lax.axis_index("tok") * shard, shard, 0)
     gain_one_grad = gain_one / norm1_late.astype(F32)

time: 875 us -> 910 us (1.040)
  waiting for transfers between devices: 400 us -> 442 us
  local copies, waits for them, and re-layouts: 50.7 us -> 23.1 us
  blocking collectives: 18.5 us -> 39 us
    reduce_scatter x4 -> x5, waiting for transfers between devices: 0.02 us -> 39.5 us  [pair_to_tok(): lax.psum_scatter(both, 'tok', scatter_dimension=0, tiled=True, axis_index...]
    all_to_all x1 -> x2, blocking collectives: 18.5 us -> 39 us  [cols_to_rows(): return lax.all_to_all(block, 'mdl', split_axis=1, concat_axis=0, tiled=True)]
    all_gather x3, waiting for transfers between devices: 58.8 us -> 69.1 us  [from_tok(): return lax.all_gather(weight, 'tok', axis=dim, tiled=True)]
    unnamed x147 -> x135, local copies, waits for them, and re-layouts: 22.6 us -> 12.3 us
    pallas_call x4 -> x5, Pallas kernels: 59.7 us -> 64.1 us  [the longest x4 56.5 us: pair_grad(): pl.pallas_call(pair_kernel, grid=(pairs,), out_shape=out_shape, in_specs=...]
    ppermute x4 -> x5, waiting for transfers between devices: 22.8 us -> 18.4 us  [pair_to_tok(): got = lax.ppermute(sent, 'tok', [(i, i ^ 1) for i in range(count)])]
    convert_element_type x4 -> x5, other arithmetic: 21.8 us -> 25.7 us  [pair_to_tok(): both = (kept.astype(F32) + got.astype(F32)).astype(BF16)]
  transfers between devices with their start and end apart: 61 -> 62, of which waited for: 37 -> 34; matrix products, arithmetic and copies ran while one was open for 17% -> 15% of each run, Pallas kernels for 16% -> 15%
where the time goes in v4:
time: 910 us; the launch traced here: 901 us
  waiting for transfers between devices  442 us (49%)
  Pallas kernels  165 us (18%)
  other arithmetic  88.6 us (10%)
  matrix products  69.7 us (8%)
  starting transfers between devices  58 us (6%)
  blocking collectives  39 us (4%)
  local copies, waits for them, and re-layouts  23.1 us (3%)
  between operations  15.8 us (2%)
    ppermute x44, waiting for transfers between devices, swap(): return lax.ppermute(block, 'mdl', [(i, i ^ distance) for i in range(size)])  277 us
    dot_general x4, matrix products, nn(): return jnp.dot(left_op, right_op, preferred_element_type=F32)  69.7 us
    all_gather x3, waiting for transfers between devices, from_tok(): return lax.all_gather(weight, 'tok', axis=dim, tiled=True)  69.1 us
    pallas_call x4, Pallas kernels, scatter_product(): pl.pallas_call(functools.partial(payload_kernel, starts), grid_spec=pltpu...  68 us
    pallas_call x4, Pallas kernels, pair_grad(): pl.pallas_call(pair_kernel, grid=(pairs,), out_shape=out_shape, in_specs=...  56.5 us
    ppermute x44, starting transfers between devices, swap(): return lax.ppermute(block, 'mdl', [(i, i ^ distance) for i in range(size)])  48.6 us
    reduce_scatter x5, waiting for transfers between devices, pair_to_tok(): lax.psum_scatter(both, 'tok', scatter_dimension=0, tiled=True, axis_index...  39.5 us
    all_to_all x2, blocking collectives, cols_to_rows(): return lax.all_to_all(block, 'mdl', split_axis=1, concat_axis=0, tiled=True)  39 us
  transfers between devices with their start and end apart: 62, of which 34 were waited for; matrix products, arithmetic and copies ran while one was open for 15% of the time, Pallas kernels for 15%

profile of v4, /device:TPU:0, one launch (start us, length us, event | category | flops | bytes accessed | tf_op | source)
XLA Modules:
  0.0 901.3 jit_solution(1188082277450769076)
XLA Ops:
  14.9 3.0 collective-permute-start
  19.4 27.3 %collective-permute-done = bf16[1024,640]{1,0:T(8,128)(2,1)S(1)} collective-permute-done((bf16[1024,640]{1,0:T(8,128)(2,1)S(1)}, bf16[1024,640]{1,0:T(8,128)(2,1)S(1)}, u32[]{:S(2)}, u32[]{:S(2)}) %collective-permute-start) | collective-permute-done | bytes 1310752 | tf_op jit(solution)/shard_map/ppermute | solution.py:38
  54.7 9.0 %collective-permute-done.2 = bf16[512,640]{1,0:T(8,128)(2,1)S(1)} collective-permute-done((bf16[512,640]{1,0:T(8,128)(2,1)}, bf16[512,640]{1,0:T(8,128)(2,1)S(1)}, u32[]{:S(2)}, u32[]{:S(2)}) %collective-permute-start.2) | collective-permute-done | bytes 655392 | tf_op jit(solution)/shard_map/ppermute | solution.py:38
  63.9 3.2 collective-permute-done.3
  70.5 15.9 %all-gather.4.cloned.1.call-done.refs_1_.weight_ref.refs_0_ = bf16[2560,1408]{1,0:T(8,128)(2,1)} async-done(((bf16[320,1408]{1,0:T(8,128)(2,1)}), bf16[2560,1408]{1,0:T(8,128)(2,1)}) %all-gather.4.cloned.1.call-update) | async-done | bytes 7208976 | tf_op jit(solution)/shard_map/all_gather | solution.py:509
  86.4 9.0 %multiply_convert_fusion.2 = bf16[1024,768]{1,0:T(8,128)(2,1)} fusion(bf16[1024,2560]{1,0:T(8,128)(2,1)} %copy-done.34, bf16[2560,1408]{1,0:T(8,128)(2,1)} %all-gather.4.cloned.1.call-done.refs_1_.weight_ref.refs_0_, f32[1024]{0:T(1024)S(1)} %add_rsqrt_fusion.1), kind=kOutput, calls=%fused_computation.28 | convolution fusion | flops 4028104704 | bytes 10752000 | tf_op jit(solution)/shard_map/dot_general | solution.py:33
  95.5 3.8 all-to-all-start
  99.3 19.8 %all-to-all-done = bf16[4,256,768]{2,1,0:T(8,128)(2,1)S(1)} async-done(((bf16[4,256,768]{2,1,0:T(8,128)(2,1)}), bf16[4,256,768]{2,1,0:T(8,128)(2,1)S(1)}, u32[]{:S(2)}, u32[]{:S(2)}) %all-to-all-start) | async-done | bytes 1572896 | tf_op jit(solution)/shard_map/all_to_all | solution.py:142
  123.9 5.7 collective-permute-done.4
  131.8 2.8 collective-permute-done.6
  136.2 10.8 %attention_forward.1 = (bf16[256,2560]{1,0:T(8,128)(2,1)S(1)}, f32[10,256,1]{2,1,0:T(8,128)S(1)}) custom-call(s32[1]{0:T(128)} %bitcast.1.first_ref, bf16[256,3072]{1,0:T(8,128)(2,1)S(1)} %bitcast.113, bf16[1024,512]{1,0:T(8,128)(2,1)S(1)} %constant_dynamic-update-slice_fusion.4.kv_ref, f32[256,128]{1,0:T(8,128)S(1)} %get-tuple-element.124.cos_ref, ...), custom_call_target="tpu_custom_call" | custom-call | flops 2684354560 | bytes 3670016 | tf_op jit(solution)/shard_map/attention_forward/pallas_call | solution.py:225
  147.2 18.4 %all_to_all.76 = bf16[256,4,640]{2,0,1:T(8,128)(2,1)} all-to-all(bf16[256,4,640]{2,0,1:T(8,128)(2,1)S(1)} %bitcast.123), channel_id=1, replica_groups=mesh['tok'=8,'mdl'=4] {'mdl'}, dimensions={1} | all-to-all | bytes 2621440 | tf_op jit(solution)/shard_map/all_to_all | solution.py:146
  165.6 7.8 shard_map.169
  174.9 25.7 %collective-permute-done.10 = bf16[2,512,640]{2,1,0:T(8,128)(2,1)S(1)} collective-permute-done((bf16[2,512,640]{2,1,0:T(8,128)(2,1)S(1)}, bf16[2,512,640]{2,1,0:T(8,128)(2,1)S(1)}, u32[]{:S(2)}, u32[]{:S(2)}) %collective-permute-start.10) | collective-permute-done | bytes 1310752 | tf_op jit(solution)/shard_map/ppermute | solution.py:38
  200.8 2.1 collective-permute-start.11
  204.3 11.3 %collective-permute-done.11 = bf16[512,640]{1,0:T(8,128)(2,1)S(1)} collective-permute-done((bf16[512,640]{1,0:T(8,128)(2,1)S(1)}, bf16[512,640]{1,0:T(8,128)(2,1)S(1)}, u32[]{:S(2)}, u32[]{:S(2)}) %collective-permute-start.11) | collective-permute-done | bytes 655392 | tf_op jit(solution)/shard_map/ppermute | solution.py:38
  220.6 26.1 %collective-permute-done.12 = bf16[1024,640]{1,0:T(8,128)(2,1)S(1)} collective-permute-done((bf16[1024,640]{1,0:T(8,128)(2,1)S(1)}, bf16[1024,640]{1,0:T(8,128)(2,1)S(1)}, u32[]{:S(2)}, u32[]{:S(2)}) %collective-permute-start.12) | collective-permute-done | bytes 1310752 | tf_op jit(solution)/shard_map/ppermute | solution.py:38
  250.7 10.2 %collective-permute-done.14 = bf16[512,640]{1,0:T(8,128)(2,1)S(1)} collective-permute-done((bf16[512,640]{1,0:T(8,128)(2,1)S(1)}, bf16[512,640]{1,0:T(8,128)(2,1)S(1)}, u32[]{:S(2)}, u32[]{:S(2)}) %collective-permute-start.14) | collective-permute-done | bytes 655392 | tf_op jit(solution)/shard_map/ppermute | solution.py:38
  262.2 3.3 fusion.1.left_ref
  265.5 17.8 %fusion.4 = f32[1024,1920]{1,0:T(8,128)} fusion(bf16[1024,2560]{1,0:T(8,128)(2,1)} %fusion.1.left_ref, bf16[2560,3840]{1,0:T(8,128)(2,1)} %all-gather.6.cloned.1.call-done.refs_2_), kind=kOutput, calls=%fused_computation.7 | convolution fusion | flops 10066329600 | bytes 22937600 | tf_op jit(solution)/shard_map/dot_general | solution.py:33
  283.3 19.4 %multiply_convert_fusion = (bf16[1024,1920]{1,0:T(8,128)(2,1)}, f32[1024,1920]{1,0:T(8,128)}) fusion(f32[1024,1920]{1,0:T(8,128)} %fusion.4, bf16[1024,2560]{1,0:T(8,128)(2,1)S(1)} %copy-done.41, bf16[2560,3840]{1,0:T(8,128)(2,1)} %all-gather.6.cloned.1.call-done.refs_2_), kind=kOutput, calls=%fused_computation.18 | convolution fusion | flops 10085990400 | bytes 34734080 | tf_op jit(solution)/shard_map/dot_general | solution.py:33
  302.7 53.1 %all-gather.8.cloned.1.call-done.refs_1_ = bf16[2560,1920]{1,0:T(8,128)(2,1)} async-done(((bf16[320,1920]{1,0:T(8,128)(2,1)}), bf16[2560,1920]{1,0:T(8,128)(2,1)}) %all-gather.8.cloned.1.call-update) | async-done | bytes 9830416 | tf_op jit(solution)/shard_map/all_gather | solution.py:509
  355.8 23.5 %fusion.53 = (bf16[1024,1920]{1,0:T(8,128)(2,1)}, f32[1024]{0:T(1024)S(1)}, bf16[1024,1920]{1,0:T(8,128)(2,1)}) fusion(f32[1024,1920]{1,0:T(8,128)} %fusion.4, f32[1024,1920]{1,0:T(8,128)} %get-tuple-element.58, bf16[1024,2560]{1,0:T(8,128)(2,1)} %left_ref.1, bf16[2560,1920]{1,0:T(8,128)(2,1)} %all-gather.8.cloned.1.call-done.refs_1_), kind=kOutput, calls=%fused_computation.150 | convolution fusion | flops 10117446656 | bytes 38670336 | tf_op jit(solution)/shard_map/dot_general | solution.py:33
  379.3 33.5 %shard_map.170 = (bf16[2,512,640]{2,1,0:T(8,128)(2,1)}, bf16[2,512,640]{2,1,0:T(8,128)(2,1)}, bf16[2,512,640]{2,1,0:T(8,128)(2,1)S(1)}, bf16[2,512,640]{2,1,0:T(8,128)(2,1)S(1)}) custom-call(s32[1]{0:T(128)} %bitcast.me_ref, bf16[1024,1920]{1,0:T(8,128)(2,1)} %get-tuple-element.99.refs_0_.right_ref, bf16[1024,1920]{1,0:T(8,128)(2,1)} %get-tuple-element.101.refs_1_.right_ref, ...), custom_call_target="tpu_custom_call" | custom-call | flops 20132659200 | bytes 32768000 | tf_op jit(solution)/shard_map/pallas_call | solution.py:410
  417.4 29.0 %collective-permute-done.20 = f32[8,128]{1,0:T(8,128)S(1)} collective-permute-done((f32[8,128]{1,0:T(8,128)S(1)}, f32[8,128]{1,0:T(8,128)S(1)}, u32[]{:S(2)}, u32[]{:S(2)}) %collective-permute-start.20) | collective-permute-done | bytes 4128 | tf_op jit(solution)/shard_map/ppermute | solution.py:38
  452.7 15.5 %shard_map.171 = (bf16[1280,1920]{1,0:T(8,128)(2,1)}, bf16[1280,1920]{1,0:T(8,128)(2,1)}) custom-call(s32[1]{0:T(128)} %bitcast.19.core_ref, bf16[1024,2560]{1,0:T(8,128)(2,1)} %fusion.1.left_ref, bf16[1024,1920]{1,0:T(8,128)(2,1)S(1)} %copy-done.23), custom_call_target="tpu_custom_call" | custom-call | flops 10066329600 | bytes 19005440 | tf_op jit(solution)/shard_map/pallas_call | solution.py:330
  471.6 4.0 fusion.54
  476.7 27.9 %collective-permute-done.26.along_x = bf16[1024,640]{1,0:T(8,128)(2,1)S(1)} collective-permute-done((bf16[1024,640]{1,0:T(8,128)(2,1)S(1)}, bf16[1024,640]{1,0:T(8,128)(2,1)S(1)}, u32[]{:S(2)}, u32[]{:S(2)}) %collective-permute-start.26) | collective-permute-done | bytes 1310752 | tf_op jit(solution)/shard_map/ppermute | solution.py:38
  505.3 2.1 collective-permute-start.29
  507.4 11.4 %collective-permute-done.28.top = bf16[512,640]{1,0:T(8,128)(2,1)S(1)} collective-permute-done((bf16[512,640]{1,0:T(8,128)(2,1)S(1)}, bf16[512,640]{1,0:T(8,128)(2,1)S(1)}, u32[]{:S(2)}, u32[]{:S(2)}) %collective-permute-start.28) | collective-permute-done | bytes 655392 | tf_op jit(solution)/shard_map/ppermute | solution.py:38
  519.2 6.6 shard_map.173
  525.8 7.6 shard_map.176
  533.4 3.7 collective-permute-done.46
  537.1 3.0 add_convert_fusion.4
  540.2 7.5 add_convert_fusion.1
  547.8 2.1 copy-done.22
  549.9 15.6 %shard_map.177 = (bf16[1280,1920]{1,0:T(8,128)(2,1)}, bf16[1280,1920]{1,0:T(8,128)(2,1)}) custom-call(s32[1]{0:T(128)} %bitcast.19.core_ref, bf16[1024,2560]{1,0:T(8,128)(2,1)} %fusion.1.left_ref, bf16[1024,1920]{1,0:T(8,128)(2,1)S(1)} %copy-done.22), custom_call_target="tpu_custom_call" | custom-call | flops 10066329600 | bytes 19005440 | tf_op jit(solution)/shard_map/pallas_call | solution.py:330
  565.5 8.4 collective-permute-done.47
  573.9 5.9 add_convert_fusion.2
  579.9 4.5 all-to-all-start.2
  584.5 17.0 %all-to-all-done.2 = bf16[4,256,640]{2,1,0:T(8,128)(2,1)} async-done(((bf16[4,256,640]{2,1,0:T(8,128)(2,1)}), bf16[4,256,640]{2,1,0:T(8,128)(2,1)}, u32[]{:S(2)}, u32[]{:S(2)}) %all-to-all-start.2) | async-done | bytes 1310752 | tf_op jit(solution)/shard_map/all_to_all | solution.py:142
  603.5 15.7 %attention_backward.1 = (bf16[256,2560]{1,0:T(8,128)(2,1)S(1)}, f32[1024,512]{1,0:T(8,128)S(1)}) custom-call(s32[1]{0:T(128)} %bitcast.1.first_ref, bf16[256,3072]{1,0:T(8,128)(2,1)S(1)} %bitcast.114, bf16[1024,512]{1,0:T(8,128)(2,1)S(1)} %copy-done.11, f32[256,128]{1,0:T(8,128)S(1)} %copy-done.17, f32[256,128]{1,0:T(8,128)S(1)} %copy-done.15, ...), custom_call_target="tpu_custom_call" | custom-call | flops 6710886400 | bytes 8388608 | tf_op jit(solution)/shard_map/attention_backward/pallas_call | solution.py:250
  621.8 5.3 collective-permute-done.30
  628.6 3.5 collective-permute-done.31
  633.7 3.5 collective-permute-done.33
  638.3 20.7 %all_to_all.77 = bf16[256,4,768]{2,0,1:T(8,128)(2,1)} all-to-all(bf16[256,4,768]{2,0,1:T(8,128)(2,1)S(1)} %bitcast.122), channel_id=1, replica_groups=mesh['tok'=8,'mdl'=4] {'mdl'}, dimensions={1} | all-to-all | bytes 3145728 | tf_op jit(solution)/shard_map/all_to_all | solution.py:146
  658.9 9.5 %shard_map.174 = (bf16[2,512,640]{2,1,0:T(8,128)(2,1)S(1)}, bf16[2,512,640]{2,1,0:T(8,128)(2,1)}, bf16[2,512,640]{2,1,0:T(8,128)(2,1)S(1)}, bf16[2,512,640]{2,1,0:T(8,128)(2,1)S(1)}) custom-call(s32[1]{0:T(128)} %bitcast.me_ref, bf16[1024,768]{1,0:T(8,128)(2,1)} %bitcast.120, bf16[2560,1408]{1,0:T(8,128)(2,1)} %all-gather.4.cloned.1.call-done.refs_1_.weight_ref.refs_0_), custom_call_target="tpu_custom_call" | custom-call | flops 4026531840 | bytes 14024704 | tf_op jit(solution)/shard_map/pallas_call | solution.py:410
  669.9 9.9 %shard_map.175 = (bf16[1280,768]{1,0:T(8,128)(2,1)S(1)}, bf16[1280,768]{1,0:T(8,128)(2,1)}, f32[2560,1]{1,0:T(8,128)S(1)}) custom-call(s32[1]{0:T(128)} %bitcast.19.core_ref, bf16[1024,2560]{1,0:T(8,128)(2,1)} %copy-done.34, bf16[1024,768]{1,0:T(8,128)(2,1)S(1)} %multiply_convert_fusion.1.right_ref, ...), custom_call_target="tpu_custom_call" | custom-call | flops 4026531840 | bytes 10747904 | tf_op jit(solution)/shard_map/pallas_call | solution.py:330
  679.8 15.5 %shard_map.178 = (bf16[1280,1920]{1,0:T(8,128)(2,1)}, bf16[1280,1920]{1,0:T(8,128)(2,1)}) custom-call(s32[1]{0:T(128)} %bitcast.19.core_ref, bf16[1024,2560]{1,0:T(8,128)(2,1)} %left_ref.1, bf16[1024,1920]{1,0:T(8,128)(2,1)S(1)} %copy-done.21), custom_call_target="tpu_custom_call" | custom-call | flops 10066329600 | bytes 19005440 | tf_op jit(solution)/shard_map/pallas_call | solution.py:330
  697.7 6.3 collective-permute-done.51
  703.9 7.5 add_convert_fusion
  711.4 17.2 %shard_map.172 = (bf16[2,512,640]{2,1,0:T(8,128)(2,1)S(1)}, bf16[2,512,640]{2,1,0:T(8,128)(2,1)S(1)}, bf16[2,512,640]{2,1,0:T(8,128)(2,1)S(1)}, bf16[2,512,640]{2,1,0:T(8,128)(2,1)S(1)}) custom-call(s32[1]{0:T(128)} %bitcast.me_ref, bf16[1024,1920]{1,0:T(8,128)(2,1)} %get-tuple-element.67.refs_0_.right_ref, ...), custom_call_target="tpu_custom_call" | custom-call | flops 10066329600 | bytes 19005440 | tf_op jit(solution)/shard_map/pallas_call | solution.py:410
  730.1 29.7 %collective-permute-done.24 = bf16[2,512,640]{2,1,0:T(8,128)(2,1)S(1)} collective-permute-done((bf16[2,512,640]{2,1,0:T(8,128)(2,1)S(1)}, bf16[2,512,640]{2,1,0:T(8,128)(2,1)S(1)}, u32[]{:S(2)}, u32[]{:S(2)}) %collective-permute-start.24) | collective-permute-done | bytes 1310752 | tf_op jit(solution)/shard_map/ppermute | solution.py:38
  768.5 10.3 %collective-permute-done.25 = bf16[512,640]{1,0:T(8,128)(2,1)} collective-permute-done((bf16[512,640]{1,0:T(8,128)(2,1)}, bf16[512,640]{1,0:T(8,128)(2,1)}, u32[]{:S(2)}, u32[]{:S(2)}) %collective-permute-start.25) | collective-permute-done | bytes 655392 | tf_op jit(solution)/shard_map/ppermute | solution.py:38
  778.9 2.8 bitcast_add_fusion.2
  787.2 19.0 %collective-permute-done.23 = bf16[512,640]{1,0:T(8,128)(2,1)S(1)} collective-permute-done((bf16[512,640]{1,0:T(8,128)(2,1)}, bf16[512,640]{1,0:T(8,128)(2,1)S(1)}, u32[]{:S(2)}, u32[]{:S(2)}) %collective-permute-start.23) | collective-permute-done | bytes 655392 | tf_op jit(solution)/shard_map/ppermute | solution.py:38
  806.1 2.6 bitcast_add_fusion.3
  813.8 2.1 fusion.27
  821.1 9.2 %collective-permute-done.37 = bf16[512,640]{1,0:T(8,128)(2,1)S(1)} collective-permute-done((bf16[512,640]{1,0:T(8,128)(2,1)}, bf16[512,640]{1,0:T(8,128)(2,1)S(1)}, u32[]{:S(2)}, u32[]{:S(2)}) %collective-permute-start.37) | collective-permute-done | bytes 655392 | tf_op jit(solution)/shard_map/ppermute | solution.py:38
  835.0 4.6 fusion.12
  841.7 5.2 convert_multiply_fusion.3
  847.7 2.1 convert_multiply_fusion.7
  851.0 39.5 %reduce-scatter.14.cloned.1.call-done = bf16[320,1920]{1,0:T(8,128)(2,1)} async-done(((bf16[1280,1920]{1,0:T(8,128)(2,1)}), bf16[320,1920]{1,0:T(8,128)(2,1)}) %reduce-scatter.14.cloned.1.call-update) | async-done | bytes 1228816 | tf_op jit(solution)/shard_map/reduce_scatter | solution.py:517
  890.5 2.9 convert_bitcast_fusion
  (327 shorter events, 106.8 us)
Async XLA Ops:
  7.2 79.2 %all-gather.4.cloned.1.call-start = ((), (), s32[]{:S(2)}) async-start(), calls=%async_computation.9 | async-start | bytes 8110080 | tf_op jit(solution)/shard_map/all_gather | solution.py:509
  11.3 254.2 %all-gather.6.cloned.1.call-start = ((), (), s32[]{:S(2)}) async-start(), calls=%async_computation.10 | async-start | bytes 22118400 | tf_op jit(solution)/shard_map/all_gather | solution.py:509
  13.6 342.2 %all-gather.8.cloned.1.call-start = ((), (), s32[]{:S(2)}) async-start(), calls=%async_computation.11 | async-start | bytes 11059200 | tf_op jit(solution)/shard_map/all_gather | solution.py:509
  14.9 31.7 %collective-permute-start = (bf16[1024,640]{1,0:T(8,128)(2,1)S(1)}, bf16[1024,640]{1,0:T(8,128)(2,1)S(1)}, u32[]{:S(2)}, u32[]{:S(2)}) collective-permute-start(bf16[1024,640]{1,0:T(8,128)(2,1)S(1)} %copy-done.30), channel_id=1, source_target_pairs={{0,1},{1,0},{2,3},{3,2},{4,5},{5,4},{6,7},{7,6},{8,9},{9,8},{10,11... | collective-permute-start | bytes 3932168 | tf_op jit(solution)/shard_map/ppermute | solution.py:38
  17.9 31.4 %collective-permute-start.1 = (bf16[1024,640]{1,0:T(8,128)(2,1)S(1)}, bf16[1024,640]{1,0:T(8,128)(2,1)S(1)}, u32[]{:S(2)}, u32[]{:S(2)}) collective-permute-start(bf16[1024,640]{1,0:T(8,128)(2,1)S(1)} %copy-done.30), channel_id=1, source_target_pairs={{0,2},{1,3},{2,0},{3,1},{4,6},{5,7},{6,4},{7,5},{8,10},{9,11},{10,... | collective-permute-start | bytes 3932168 | tf_op jit(solution)/shard_map/ppermute | solution.py:38
  47.5 16.2 %collective-permute-start.2 = (bf16[512,640]{1,0:T(8,128)(2,1)}, bf16[512,640]{1,0:T(8,128)(2,1)S(1)}, u32[]{:S(2)}, u32[]{:S(2)}) collective-permute-start(bf16[512,640]{1,0:T(8,128)(2,1)} %slice.220), channel_id=1, source_target_pairs={{0,2},{1,3},{2,0},{3,1},{4,6},{5,7},{6,4},{7,5},{8,10},{9,11},{10,... | collective-permute-start | bytes 1966088 | tf_op jit(solution)/shard_map/ppermute | solution.py:38
  51.3 15.8 %collective-permute-start.3 = (bf16[512,640]{1,0:T(8,128)(2,1)}, bf16[512,640]{1,0:T(8,128)(2,1)}, u32[]{:S(2)}, u32[]{:S(2)}) collective-permute-start(bf16[512,640]{1,0:T(8,128)(2,1)} %slice.221), channel_id=1, source_target_pairs={{0,1},{1,0},{2,3},{3,2},{4,5},{5,4},{6,7},{7,6},{8,9},{9,8},{10,11... | collective-permute-start | bytes 1966088 | tf_op jit(solution)/shard_map/ppermute | solution.py:38
  95.5 23.6 %all-to-all-start = ((bf16[4,256,768]{2,1,0:T(8,128)(2,1)}), bf16[4,256,768]{2,1,0:T(8,128)(2,1)S(1)}, u32[]{:S(2)}, u32[]{:S(2)}) async-start(bf16[4,256,768]{2,1,0:T(8,128)(2,1)} %bitcast.3), calls=%async_computation | async-start | bytes 3145728 | tf_op jit(solution)/shard_map/all_to_all | solution.py:142
  99.3 740.4 %reduce-scatter.8.cloned.1.call-start = ((), (), s32[]{:S(2)}) async-start(), calls=%async_computation.13 | async-start | bytes 2048000 | tf_op jit(solution)/shard_map/reduce_scatter | solution.py:517
  121.7 7.8 collective-permute-start.4
  123.1 8.0 collective-permute-start.5
  129.6 5.0 collective-permute-start.6
  131.1 5.0 collective-permute-start.7
  173.4 27.2 %collective-permute-start.10 = (bf16[2,512,640]{2,1,0:T(8,128)(2,1)S(1)}, bf16[2,512,640]{2,1,0:T(8,128)(2,1)S(1)}, u32[]{:S(2)}, u32[]{:S(2)}) collective-permute-start(bf16[2,512,640]{2,1,0:T(8,128)(2,1)S(1)} %get-tuple-element.56), channel_id=1, source_target_pairs={{0,2},{1,3},{2,0},{3,1},{4,6},{5,7},{6,4},{7,5},{8,10},{9,11},{10,... | collective-permute-start | bytes 3932168 | tf_op jit(solution)/shard_map/ppermute | solution.py:38
  174.5 29.6 %collective-permute-start.8 = (bf16[2,512,640]{2,1,0:T(8,128)(2,1)S(1)}, bf16[2,512,640]{2,1,0:T(8,128)(2,1)S(1)}, u32[]{:S(2)}, u32[]{:S(2)}) collective-permute-start(bf16[2,512,640]{2,1,0:T(8,128)(2,1)S(1)} %get-tuple-element.54), channel_id=1, source_target_pairs={{0,1},{1,0},{2,3},{3,2},{4,5},{5,4},{6,7},{7,6},{8,9},{9,8},{10,11... | collective-permute-start | bytes 3932168 | tf_op jit(solution)/shard_map/ppermute | solution.py:38
  200.8 14.8 %collective-permute-start.11 = (bf16[512,640]{1,0:T(8,128)(2,1)S(1)}, bf16[512,640]{1,0:T(8,128)(2,1)S(1)}, u32[]{:S(2)}, u32[]{:S(2)}) collective-permute-start(bf16[512,640]{1,0:T(8,128)(2,1)S(1)} %fusion.21), channel_id=1, source_target_pairs={{0,1},{1,0},{2,3},{3,2},{4,5},{5,4},{6,7},{7,6},{8,9},{9,8},{10,11... | collective-permute-start | bytes 1966088 | tf_op jit(solution)/shard_map/ppermute | solution.py:38
  204.2 11.6 %collective-permute-start.9 = (bf16[512,640]{1,0:T(8,128)(2,1)S(1)}, bf16[512,640]{1,0:T(8,128)(2,1)S(1)}, u32[]{:S(2)}, u32[]{:S(2)}) collective-permute-start(bf16[512,640]{1,0:T(8,128)(2,1)S(1)} %fusion.20), channel_id=1, source_target_pairs={{0,2},{1,3},{2,0},{3,1},{4,6},{5,7},{6,4},{7,5},{8,10},{9,11},{10,... | collective-permute-start | bytes 1966088 | tf_op jit(solution)/shard_map/ppermute | solution.py:38
  218.5 28.2 %collective-permute-start.12 = (bf16[1024,640]{1,0:T(8,128)(2,1)S(1)}, bf16[1024,640]{1,0:T(8,128)(2,1)S(1)}, u32[]{:S(2)}, u32[]{:S(2)}) collective-permute-start(bf16[1024,640]{1,0:T(8,128)(2,1)S(1)} %get-tuple-element.98), channel_id=1, source_target_pairs={{0,1},{1,0},{2,3},{3,2},{4,5},{5,4},{6,7},{7,6},{8,9},{9,8},{10,11... | collective-permute-start | bytes 3932168 | tf_op jit(solution)/shard_map/ppermute | solution.py:38
  219.2 29.3 %collective-permute-start.13 = (bf16[1024,640]{1,0:T(8,128)(2,1)S(1)}, bf16[1024,640]{1,0:T(8,128)(2,1)S(1)}, u32[]{:S(2)}, u32[]{:S(2)}) collective-permute-start(bf16[1024,640]{1,0:T(8,128)(2,1)S(1)} %get-tuple-element.98), channel_id=1, source_target_pairs={{0,2},{1,3},{2,0},{3,1},{4,6},{5,7},{6,4},{7,5},{8,10},{9,11},{10,... | collective-permute-start | bytes 3932168 | tf_op jit(solution)/shard_map/ppermute | solution.py:38
  246.8 14.1 %collective-permute-start.14 = (bf16[512,640]{1,0:T(8,128)(2,1)S(1)}, bf16[512,640]{1,0:T(8,128)(2,1)S(1)}, u32[]{:S(2)}, u32[]{:S(2)}) collective-permute-start(bf16[512,640]{1,0:T(8,128)(2,1)S(1)} %slice.233), channel_id=1, source_target_pairs={{0,2},{1,3},{2,0},{3,1},{4,6},{5,7},{6,4},{7,5},{8,10},{9,11},{10,... | collective-permute-start | bytes 1966088 | tf_op jit(solution)/shard_map/ppermute | solution.py:38
  248.5 12.5 %collective-permute-start.15 = (bf16[512,640]{1,0:T(8,128)(2,1)S(1)}, bf16[512,640]{1,0:T(8,128)(2,1)S(1)}, u32[]{:S(2)}, u32[]{:S(2)}) collective-permute-start(bf16[512,640]{1,0:T(8,128)(2,1)S(1)} %slice.234), channel_id=1, source_target_pairs={{0,1},{1,0},{2,3},{3,2},{4,5},{5,4},{6,7},{7,6},{8,9},{9,8},{10,11... | collective-permute-start | bytes 1966088 | tf_op jit(solution)/shard_map/ppermute | solution.py:38
  413.9 33.0 %collective-permute-start.18 = (bf16[2,512,640]{2,1,0:T(8,128)(2,1)}, bf16[2,512,640]{2,1,0:T(8,128)(2,1)}, u32[]{:S(2)}, u32[]{:S(2)}) collective-permute-start(bf16[2,512,640]{2,1,0:T(8,128)(2,1)} %get-tuple-element.63), channel_id=1, source_target_pairs={{0,2},{1,3},{2,0},{3,1},{4,6},{5,7},{6,4},{7,5},{8,10},{9,11},{10,... | collective-permute-start | bytes 3932168 | tf_op jit(solution)/shard_map/ppermute | solution.py:38
  415.3 34.6 %collective-permute-start.16 = (bf16[2,512,640]{2,1,0:T(8,128)(2,1)}, bf16[2,512,640]{2,1,0:T(8,128)(2,1)}, u32[]{:S(2)}, u32[]{:S(2)}) collective-permute-start(bf16[2,512,640]{2,1,0:T(8,128)(2,1)} %get-tuple-element.61), channel_id=1, source_target_pairs={{0,1},{1,0},{2,3},{3,2},{4,5},{5,4},{6,7},{7,6},{8,9},{9,8},{10,11... | collective-permute-start | bytes 3932168 | tf_op jit(solution)/shard_map/ppermute | solution.py:38
  416.8 29.5 %collective-permute-start.20 = (f32[8,128]{1,0:T(8,128)S(1)}, f32[8,128]{1,0:T(8,128)S(1)}, u32[]{:S(2)}, u32[]{:S(2)}) collective-permute-start(f32[8,128]{1,0:T(8,128)S(1)} %bitcast.129), channel_id=1, source_target_pairs={{0,1},{1,0},{2,3},{3,2},{4,5},{5,4},{6,7},{7,6},{8,9},{9,8},{10,11... | collective-permute-start | bytes 12296 | tf_op jit(solution)/shard_map/ppermute | solution.py:38
  446.3 21.8 %collective-permute-start.21 = (f32[8,128]{1,0:T(8,128)S(1)}, f32[8,128]{1,0:T(8,128)S(1)}, u32[]{:S(2)}, u32[]{:S(2)}) collective-permute-start(f32[8,128]{1,0:T(8,128)S(1)} %bitcast_add_fusion.8), channel_id=1, source_target_pairs={{0,2},{1,3},{2,0},{3,1},{4,6},{5,7},{6,4},{7,5},{8,10},{9,11},{10,... | collective-permute-start | bytes 12296 | tf_op jit(solution)/shard_map/ppermute | solution.py:38
  448.3 19.8 %collective-permute-start.19 = (bf16[512,640]{1,0:T(8,128)(2,1)S(1)}, bf16[512,640]{1,0:T(8,128)(2,1)S(1)}, u32[]{:S(2)}, u32[]{:S(2)}) collective-permute-start(bf16[512,640]{1,0:T(8,128)(2,1)S(1)} %fusion.23), channel_id=1, source_target_pairs={{0,1},{1,0},{2,3},{3,2},{4,5},{5,4},{6,7},{7,6},{8,9},{9,8},{10,11... | collective-permute-start | bytes 1966088 | tf_op jit(solution)/shard_map/ppermute | solution.py:38
  451.1 18.6 %collective-permute-start.17 = (bf16[512,640]{1,0:T(8,128)(2,1)S(1)}, bf16[512,640]{1,0:T(8,128)(2,1)S(1)}, u32[]{:S(2)}, u32[]{:S(2)}) collective-permute-start(bf16[512,640]{1,0:T(8,128)(2,1)S(1)} %fusion.22), channel_id=1, source_target_pairs={{0,2},{1,3},{2,0},{3,1},{4,6},{5,7},{6,4},{7,5},{8,10},{9,11},{10,... | collective-permute-start | bytes 1966088 | tf_op jit(solution)/shard_map/ppermute | solution.py:38
  469.7 49.5 %slice-start = ((s8[7208960]{0:T(1024)(128)(4,1)}), s8[4194304]{0:T(1024)(128)(4,1)S(1)}, s32[]{:S(2)}) async-start(s8[7208960]{0:T(1024)(128)(4,1)} %bitcast.110), calls=%async_computation.17 | async-start | bytes 8388608
  471.6 47.6 %slice-start.1 = ((s8[7208960]{0:T(1024)(128)(4,1)}), s8[3014656]{0:T(1024)(128)(4,1)S(1)}, s32[]{:S(2)}) async-start(s8[7208960]{0:T(1024)(128)(4,1)} %bitcast.110), calls=%async_computation.18 | async-start | bytes 6029312
  475.6 29.0 %collective-permute-start.26 = (bf16[1024,640]{1,0:T(8,128)(2,1)S(1)}, bf16[1024,640]{1,0:T(8,128)(2,1)S(1)}, u32[]{:S(2)}, u32[]{:S(2)}) collective-permute-start(bf16[1024,640]{1,0:T(8,128)(2,1)S(1)} %get-tuple-element.66.own), channel_id=1, source_target_pairs={{0,1},{1,0},{2,3},{3,2},{4,5},{5,4},{6,7},{7,6},{8,9},{9,8},{10,11... | collective-permute-start | bytes 3932168 | tf_op jit(solution)/shard_map/ppermute | solution.py:38
  476.2 29.1 %collective-permute-start.27 = (bf16[1024,640]{1,0:T(8,128)(2,1)S(1)}, bf16[1024,640]{1,0:T(8,128)(2,1)S(1)}, u32[]{:S(2)}, u32[]{:S(2)}) collective-permute-start(bf16[1024,640]{1,0:T(8,128)(2,1)S(1)} %get-tuple-element.66.own), channel_id=1, source_target_pairs={{0,2},{1,3},{2,0},{3,1},{4,6},{5,7},{6,4},{7,5},{8,10},{9,11},{10,... | collective-permute-start | bytes 3932168 | tf_op jit(solution)/shard_map/ppermute | solution.py:38
  504.6 14.3 %collective-permute-start.28 = (bf16[512,640]{1,0:T(8,128)(2,1)S(1)}, bf16[512,640]{1,0:T(8,128)(2,1)S(1)}, u32[]{:S(2)}, u32[]{:S(2)}) collective-permute-start(bf16[512,640]{1,0:T(8,128)(2,1)S(1)} %slice.245), channel_id=1, source_target_pairs={{0,2},{1,3},{2,0},{3,1},{4,6},{5,7},{6,4},{7,5},{8,10},{9,11},{10,... | collective-permute-start | bytes 1966088 | tf_op jit(solution)/shard_map/ppermute | solution.py:38
  505.3 13.9 %collective-permute-start.29 = (bf16[512,640]{1,0:T(8,128)(2,1)S(1)}, bf16[512,640]{1,0:T(8,128)(2,1)S(1)}, u32[]{:S(2)}, u32[]{:S(2)}) collective-permute-start(bf16[512,640]{1,0:T(8,128)(2,1)S(1)} %slice.246), channel_id=1, source_target_pairs={{0,1},{1,0},{2,3},{3,2},{4,5},{5,4},{6,7},{7,6},{8,9},{9,8},{10,11... | collective-permute-start | bytes 1966088 | tf_op jit(solution)/shard_map/ppermute | solution.py:38
  507.4 32.8 %collective-permute-start.48 = (bf16[1280,1920]{1,0:T(8,128)(2,1)}, bf16[1280,1920]{1,0:T(8,128)(2,1)}, u32[]{:S(2)}, u32[]{:S(2)}) collective-permute-start(bf16[1280,1920]{1,0:T(8,128)(2,1)} %get-tuple-element.91), channel_id=1, source_target_pairs={{0,4},{4,0},{8,12},{12,8},{16,20},{20,16},{24,28},{28,24},{1,5},{5... | collective-permute-start | bytes 14745608 | tf_op jit(solution)/shard_map/ppermute | solution.py:514
  533.4 3.7 collective-permute-start.46
  540.2 301.5 %reduce-scatter.12.cloned.1.call-start = ((), (), s32[]{:S(2)}) async-start(), calls=%async_computation.15 | async-start | bytes 6144000 | tf_op jit(solution)/shard_map/reduce_scatter | solution.py:517
  547.7 293.9 %reduce-scatter.10.cloned.1.call-start = ((), (), s32[]{:S(2)}) async-start(), calls=%async_computation.14 | async-start | bytes 6144000 | tf_op jit(solution)/shard_map/reduce_scatter | solution.py:517
  565.5 8.4 collective-permute-start.47
  579.9 21.6 %all-to-all-start.2 = ((bf16[4,256,640]{2,1,0:T(8,128)(2,1)}), bf16[4,256,640]{2,1,0:T(8,128)(2,1)}, u32[]{:S(2)}, u32[]{:S(2)}) async-start(bf16[4,256,640]{2,1,0:T(8,128)(2,1)} %bitcast.24), calls=%async_computation.2 | async-start | bytes 2621440 | tf_op jit(solution)/shard_map/all_to_all | solution.py:142
  584.4 263.3 %reduce-scatter.6.cloned.1.call-start = ((), (), s32[]{:S(2)}) async-start(), calls=%async_computation.12 | async-start | bytes 2457600 | tf_op jit(solution)/shard_map/reduce_scatter | solution.py:517
  619.5 7.6 collective-permute-start.30
  621.0 7.6 collective-permute-start.32
  627.1 5.0 collective-permute-start.31
  632.2 5.0 collective-permute-start.33
  679.8 16.0 %collective-permute-start.45 = (bf16[1280,768]{1,0:T(8,128)(2,1)}, bf16[1280,768]{1,0:T(8,128)(2,1)S(1)}, u32[]{:S(2)}, u32[]{:S(2)}) collective-permute-start(bf16[1280,768]{1,0:T(8,128)(2,1)} %get-tuple-element.83), channel_id=1, source_target_pairs={{0,4},{4,0},{8,12},{12,8},{16,20},{20,16},{24,28},{28,24},{1,5},{5... | collective-permute-start | bytes 5898248 | tf_op jit(solution)/shard_map/ppermute | solution.py:514
  695.3 8.6 collective-permute-start.51
  697.6 192.9 %reduce-scatter.14.cloned.1.call-start = ((), (), s32[]{:S(2)}) async-start(), calls=%async_computation.16 | async-start | bytes 6144000 | tf_op jit(solution)/shard_map/reduce_scatter | solution.py:517
  728.6 31.1 %collective-permute-start.24 = (bf16[2,512,640]{2,1,0:T(8,128)(2,1)S(1)}, bf16[2,512,640]{2,1,0:T(8,128)(2,1)S(1)}, u32[]{:S(2)}, u32[]{:S(2)}) collective-permute-start(bf16[2,512,640]{2,1,0:T(8,128)(2,1)S(1)} %get-tuple-element.71), channel_id=1, source_target_pairs={{0,2},{1,3},{2,0},{3,1},{4,6},{5,7},{6,4},{7,5},{8,10},{9,11},{10,... | collective-permute-start | bytes 3932168 | tf_op jit(solution)/shard_map/ppermute | solution.py:38
  729.3 33.1 %collective-permute-start.22 = (bf16[2,512,640]{2,1,0:T(8,128)(2,1)S(1)}, bf16[2,512,640]{2,1,0:T(8,128)(2,1)S(1)}, u32[]{:S(2)}, u32[]{:S(2)}) collective-permute-start(bf16[2,512,640]{2,1,0:T(8,128)(2,1)S(1)} %get-tuple-element.69), channel_id=1, source_target_pairs={{0,1},{1,0},{2,3},{3,2},{4,5},{5,4},{6,7},{7,6},{8,9},{9,8},{10,11... | collective-permute-start | bytes 3932168 | tf_op jit(solution)/shard_map/ppermute | solution.py:38
  760.9 17.9 %collective-permute-start.25 = (bf16[512,640]{1,0:T(8,128)(2,1)}, bf16[512,640]{1,0:T(8,128)(2,1)}, u32[]{:S(2)}, u32[]{:S(2)}) collective-permute-start(bf16[512,640]{1,0:T(8,128)(2,1)} %fusion.25), channel_id=1, source_target_pairs={{0,1},{1,0},{2,3},{3,2},{4,5},{5,4},{6,7},{7,6},{8,9},{9,8},{10,11... | collective-permute-start | bytes 1966088 | tf_op jit(solution)/shard_map/ppermute | solution.py:38
  761.8 52.0 %collective-permute-start.36 = (bf16[2,512,640]{2,1,0:T(8,128)(2,1)}, bf16[2,512,640]{2,1,0:T(8,128)(2,1)}, u32[]{:S(2)}, u32[]{:S(2)}) collective-permute-start(bf16[2,512,640]{2,1,0:T(8,128)(2,1)} %get-tuple-element.78), channel_id=1, source_target_pairs={{0,2},{1,3},{2,0},{3,1},{4,6},{5,7},{6,4},{7,5},{8,10},{9,11},{10,... | collective-permute-start | bytes 3932168 | tf_op jit(solution)/shard_map/ppermute | solution.py:38
  763.6 42.5 %collective-permute-start.23 = (bf16[512,640]{1,0:T(8,128)(2,1)}, bf16[512,640]{1,0:T(8,128)(2,1)S(1)}, u32[]{:S(2)}, u32[]{:S(2)}) collective-permute-start(bf16[512,640]{1,0:T(8,128)(2,1)} %fusion.24), channel_id=1, source_target_pairs={{0,2},{1,3},{2,0},{3,1},{4,6},{5,7},{6,4},{7,5},{8,10},{9,11},{10,... | collective-permute-start | bytes 1966088 | tf_op jit(solution)/shard_map/ppermute | solution.py:38
  766.3 50.6 %collective-permute-start.34 = (bf16[2,512,640]{2,1,0:T(8,128)(2,1)}, bf16[2,512,640]{2,1,0:T(8,128)(2,1)}, u32[]{:S(2)}, u32[]{:S(2)}) collective-permute-start(bf16[2,512,640]{2,1,0:T(8,128)(2,1)} %copy-done.18), channel_id=1, source_target_pairs={{0,1},{1,0},{2,3},{3,2},{4,5},{5,4},{6,7},{7,6},{8,9},{9,8},{10,11... | collective-permute-start | bytes 3932168 | tf_op jit(solution)/shard_map/ppermute | solution.py:38
  768.5 13.1 %collective-permute-start.40 = (f32[8,320]{1,0:T(8,128)}, f32[8,320]{1,0:T(8,128)S(1)}, u32[]{:S(2)}, u32[]{:S(2)}) collective-permute-start(f32[8,320]{1,0:T(8,128)} %reshape.172), channel_id=1, source_target_pairs={{0,4},{4,0},{8,12},{12,8},{16,20},{20,16},{24,28},{28,24},{1,5},{5... | collective-permute-start | bytes 30728 | tf_op jit(solution)/shard_map/ppermute | solution.py:136
  781.7 4.6 collective-permute-start.41
  783.9 25.8 %collective-permute-start.38 = (f32[4,256]{1,0:T(4,128)S(1)}, f32[4,256]{1,0:T(4,128)}, u32[]{:S(2)}, u32[]{:S(2)}) collective-permute-start(f32[4,256]{1,0:T(4,128)S(1)} %dynamic_update_slice.65), channel_id=1, source_target_pairs={{0,1},{1,0},{2,3},{3,2},{4,5},{5,4},{6,7},{7,6},{8,9},{9,8},{10,11... | collective-permute-start | bytes 12296 | tf_op jit(solution)/shard_map/ppermute | solution.py:38
  787.0 21.7 %collective-permute-start.42 = (f32[8,320]{1,0:T(8,128)S(1)}, f32[8,320]{1,0:T(8,128)S(1)}, u32[]{:S(2)}, u32[]{:S(2)}) collective-permute-start(f32[8,320]{1,0:T(8,128)S(1)} %add.398), channel_id=1, source_target_pairs={{0,16},{4,20},{8,24},{12,28},{16,0},{20,4},{24,8},{28,12},{1,17},{... | collective-permute-start | bytes 30728 | tf_op jit(solution)/shard_map/ppermute | solution.py:136
  808.7 4.1 collective-permute-start.43
  811.7 7.9 collective-permute-start.39
  812.8 7.6 collective-permute-start.44
  815.8 14.5 %collective-permute-start.37 = (bf16[512,640]{1,0:T(8,128)(2,1)}, bf16[512,640]{1,0:T(8,128)(2,1)S(1)}, u32[]{:S(2)}, u32[]{:S(2)}) collective-permute-start(bf16[512,640]{1,0:T(8,128)(2,1)} %fusion.27), channel_id=1, source_target_pairs={{0,1},{1,0},{2,3},{3,2},{4,5},{5,4},{6,7},{7,6},{8,9},{9,8},{10,11... | collective-permute-start | bytes 1966088 | tf_op jit(solution)/shard_map/ppermute | solution.py:38
  819.0 14.5 %collective-permute-start.35 = (bf16[512,640]{1,0:T(8,128)(2,1)}, bf16[512,640]{1,0:T(8,128)(2,1)}, u32[]{:S(2)}, u32[]{:S(2)}) collective-permute-start(bf16[512,640]{1,0:T(8,128)(2,1)} %fusion.26), channel_id=1, source_target_pairs={{0,2},{1,3},{2,0},{3,1},{4,6},{5,7},{6,4},{7,5},{8,10},{9,11},{10,... | collective-permute-start | bytes 1966088 | tf_op jit(solution)/shard_map/ppermute | solution.py:38
  846.9 3.6 collective-permute-start.49
  850.5 42.9 %collective-permute-start.50 = (f32[320]{0:T(512)S(1)}, f32[320]{0:T(512)S(1)}, u32[]{:S(2)}, u32[]{:S(2)}) collective-permute-start(f32[320]{0:T(512)S(1)} %add.408), channel_id=1, source_target_pairs={{0,2},{1,3},{2,0},{3,1},{4,6},{5,7},{6,4},{7,5},{8,10},{9,11},{10,... | collective-permute-start | bytes 3848 | tf_op jit(solution)/shard_map/ppermute | solution.py:38
  (65 other events, 809.9 us)
Sparse Core Ops, SparseCore 0:
  11.4 74.9 all-gather.3
  88.7 173.2 all-gather.5
  263.6 92.1 all-gather.7
  540.3 33.8 reduce-scatter.7
  576.4 87.3 reduce-scatter.11
  666.0 88.9 reduce-scatter.9
  757.9 42.6 reduce-scatter.5
  802.9 87.5 reduce-scatter.13

commit v5 on v4

--- a/solution.py
+++ b/solution.py
@@ -557,7 +557,7 @@
     gelu, slope = gelu_parts(gate_in)
 
     down_local = pair_grad(cotangent, hidden)
-    down_grad = pair_to_tok(down_local).T
+    down_grad = pair_to_tok(down_local)
     d_hidden = nn(cotangent, w_down_t)
     d_gate_f = d_hidden * up_in * slope
     d_up_f = d_hidden * gelu
@@ -587,7 +587,7 @@
         d_mixed_rows = gather_mdl(d_mixed_b, 1)
         d_head = nn(d_mixed_rows, w_attn[:, qkv_cols:]).astype(BF16)
         out_local = pair_grad(d_mixed_rows, head_block)
-    out_grad = pair_to_tok(out_local).T
+    out_grad = pair_to_tok(out_local)
     d_attended = rows_to_cols(d_head)
     block_out = (mixed + ffn_scatter(ffn_payload)).astype(BF16)
     d_query, d_kv = attention_backward(
@@ -619,6 +619,8 @@
         gate_late.astype(F32) * gate_sum + up_late.astype(F32) * up_sum, axis=1
     )
     gate_grad, up_grad = unfold(gate_sum, norm2_late), unfold(up_sum, norm2_late)
+    down_grad = down_grad.T
+    out_grad = out_grad.T
     gain_two_grad = sum_mdl(gain_two)
     gain_one = sum_mdl(sum_tok(gain_one.reshape(8, -1))).reshape(-1)
     shard = norm1_gain.shape[0]

time: 910 us -> 910 us (level)
  no operation moved by 1% of the time
where the time goes in v5:
time: 910 us; the launch traced here: 901 us
  waiting for transfers between devices  442 us (49%)
  Pallas kernels  165 us (18%)
  other arithmetic  88.6 us (10%)
  matrix products  69.7 us (8%)
  starting transfers between devices  58 us (6%)
  blocking collectives  39 us (4%)
  local copies, waits for them, and re-layouts  23.1 us (3%)
  between operations  15.8 us (2%)
    ppermute x44, waiting for transfers between devices, swap(): return lax.ppermute(block, 'mdl', [(i, i ^ distance) for i in range(size)])  277 us
    dot_general x4, matrix products, nn(): return jnp.dot(left_op, right_op, preferred_element_type=F32)  69.7 us
    all_gather x3, waiting for transfers between devices, from_tok(): return lax.all_gather(weight, 'tok', axis=dim, tiled=True)  69.1 us
    pallas_call x4, Pallas kernels, scatter_product(): pl.pallas_call(functools.partial(payload_kernel, starts), grid_spec=pltpu...  68 us
    pallas_call x4, Pallas kernels, pair_grad(): pl.pallas_call(pair_kernel, grid=(pairs,), out_shape=out_shape, in_specs=...  56.5 us
    ppermute x44, starting transfers between devices, swap(): return lax.ppermute(block, 'mdl', [(i, i ^ distance) for i in range(size)])  48.6 us
    reduce_scatter x5, waiting for transfers between devices, pair_to_tok(): lax.psum_scatter(both, 'tok', scatter_dimension=0, tiled=True, axis_index...  39.5 us
    all_to_all x2, blocking collectives, cols_to_rows(): return lax.all_to_all(block, 'mdl', split_axis=1, concat_axis=0, tiled=True)  39 us
  transfers between devices with their start and end apart: 62, of which 34 were waited for; matrix products, arithmetic and copies ran while one was open for 15% of the time, Pallas kernels for 15%

profile of v5, /device:TPU:0, one launch (start us, length us, event | category | flops | bytes accessed | tf_op | source)
XLA Modules:
  0.0 901.3 jit_solution(1188082277450769076)
XLA Ops:
  14.9 3.0 collective-permute-start
  19.4 27.3 %collective-permute-done = bf16[1024,640]{1,0:T(8,128)(2,1)S(1)} collective-permute-done((bf16[1024,640]{1,0:T(8,128)(2,1)S(1)}, bf16[1024,640]{1,0:T(8,128)(2,1)S(1)}, u32[]{:S(2)}, u32[]{:S(2)}) %collective-permute-start) | collective-permute-done | bytes 1310752 | tf_op jit(solution)/shard_map/ppermute | solution.py:38
  54.7 9.0 %collective-permute-done.2 = bf16[512,640]{1,0:T(8,128)(2,1)S(1)} collective-permute-done((bf16[512,640]{1,0:T(8,128)(2,1)}, bf16[512,640]{1,0:T(8,128)(2,1)S(1)}, u32[]{:S(2)}, u32[]{:S(2)}) %collective-permute-start.2) | collective-permute-done | bytes 655392 | tf_op jit(solution)/shard_map/ppermute | solution.py:38
  63.9 3.2 collective-permute-done.3
  70.5 15.9 %all-gather.4.cloned.1.call-done.refs_1_.weight_ref.refs_0_ = bf16[2560,1408]{1,0:T(8,128)(2,1)} async-done(((bf16[320,1408]{1,0:T(8,128)(2,1)}), bf16[2560,1408]{1,0:T(8,128)(2,1)}) %all-gather.4.cloned.1.call-update) | async-done | bytes 7208976 | tf_op jit(solution)/shard_map/all_gather | solution.py:509
  86.4 9.0 %multiply_convert_fusion.2 = bf16[1024,768]{1,0:T(8,128)(2,1)} fusion(bf16[1024,2560]{1,0:T(8,128)(2,1)} %copy-done.34, bf16[2560,1408]{1,0:T(8,128)(2,1)} %all-gather.4.cloned.1.call-done.refs_1_.weight_ref.refs_0_, f32[1024]{0:T(1024)S(1)} %add_rsqrt_fusion.1), kind=kOutput, calls=%fused_computation.28 | convolution fusion | flops 4028104704 | bytes 10752000 | tf_op jit(solution)/shard_map/dot_general | solution.py:33
  95.5 3.8 all-to-all-start
  99.3 19.8 %all-to-all-done = bf16[4,256,768]{2,1,0:T(8,128)(2,1)S(1)} async-done(((bf16[4,256,768]{2,1,0:T(8,128)(2,1)}), bf16[4,256,768]{2,1,0:T(8,128)(2,1)S(1)}, u32[]{:S(2)}, u32[]{:S(2)}) %all-to-all-start) | async-done | bytes 1572896 | tf_op jit(solution)/shard_map/all_to_all | solution.py:142
  123.9 5.7 collective-permute-done.4
  131.8 2.8 collective-permute-done.6
  136.2 10.8 %attention_forward.1 = (bf16[256,2560]{1,0:T(8,128)(2,1)S(1)}, f32[10,256,1]{2,1,0:T(8,128)S(1)}) custom-call(s32[1]{0:T(128)} %bitcast.1.first_ref, bf16[256,3072]{1,0:T(8,128)(2,1)S(1)} %bitcast.113, bf16[1024,512]{1,0:T(8,128)(2,1)S(1)} %constant_dynamic-update-slice_fusion.4.kv_ref, f32[256,128]{1,0:T(8,128)S(1)} %get-tuple-element.124.cos_ref, ...), custom_call_target="tpu_custom_call" | custom-call | flops 2684354560 | bytes 3670016 | tf_op jit(solution)/shard_map/attention_forward/pallas_call | solution.py:225
  147.2 18.4 %all_to_all.76 = bf16[256,4,640]{2,0,1:T(8,128)(2,1)} all-to-all(bf16[256,4,640]{2,0,1:T(8,128)(2,1)S(1)} %bitcast.123), channel_id=1, replica_groups=mesh['tok'=8,'mdl'=4] {'mdl'}, dimensions={1} | all-to-all | bytes 2621440 | tf_op jit(solution)/shard_map/all_to_all | solution.py:146
  165.6 7.8 shard_map.169
  174.9 25.7 %collective-permute-done.10 = bf16[2,512,640]{2,1,0:T(8,128)(2,1)S(1)} collective-permute-done((bf16[2,512,640]{2,1,0:T(8,128)(2,1)S(1)}, bf16[2,512,640]{2,1,0:T(8,128)(2,1)S(1)}, u32[]{:S(2)}, u32[]{:S(2)}) %collective-permute-start.10) | collective-permute-done | bytes 1310752 | tf_op jit(solution)/shard_map/ppermute | solution.py:38
  200.8 2.1 collective-permute-start.11
  204.3 11.3 %collective-permute-done.11 = bf16[512,640]{1,0:T(8,128)(2,1)S(1)} collective-permute-done((bf16[512,640]{1,0:T(8,128)(2,1)S(1)}, bf16[512,640]{1,0:T(8,128)(2,1)S(1)}, u32[]{:S(2)}, u32[]{:S(2)}) %collective-permute-start.11) | collective-permute-done | bytes 655392 | tf_op jit(solution)/shard_map/ppermute | solution.py:38
  220.6 26.1 %collective-permute-done.12 = bf16[1024,640]{1,0:T(8,128)(2,1)S(1)} collective-permute-done((bf16[1024,640]{1,0:T(8,128)(2,1)S(1)}, bf16[1024,640]{1,0:T(8,128)(2,1)S(1)}, u32[]{:S(2)}, u32[]{:S(2)}) %collective-permute-start.12) | collective-permute-done | bytes 1310752 | tf_op jit(solution)/shard_map/ppermute | solution.py:38
  250.7 10.2 %collective-permute-done.14 = bf16[512,640]{1,0:T(8,128)(2,1)S(1)} collective-permute-done((bf16[512,640]{1,0:T(8,128)(2,1)S(1)}, bf16[512,640]{1,0:T(8,128)(2,1)S(1)}, u32[]{:S(2)}, u32[]{:S(2)}) %collective-permute-start.14) | collective-permute-done | bytes 655392 | tf_op jit(solution)/shard_map/ppermute | solution.py:38
  262.2 3.3 fusion.1.left_ref
  265.5 17.8 %fusion.4 = f32[1024,1920]{1,0:T(8,128)} fusion(bf16[1024,2560]{1,0:T(8,128)(2,1)} %fusion.1.left_ref, bf16[2560,3840]{1,0:T(8,128)(2,1)} %all-gather.6.cloned.1.call-done.refs_2_), kind=kOutput, calls=%fused_computation.7 | convolution fusion | flops 10066329600 | bytes 22937600 | tf_op jit(solution)/shard_map/dot_general | solution.py:33
  283.3 19.4 %multiply_convert_fusion = (bf16[1024,1920]{1,0:T(8,128)(2,1)}, f32[1024,1920]{1,0:T(8,128)}) fusion(f32[1024,1920]{1,0:T(8,128)} %fusion.4, bf16[1024,2560]{1,0:T(8,128)(2,1)S(1)} %copy-done.41, bf16[2560,3840]{1,0:T(8,128)(2,1)} %all-gather.6.cloned.1.call-done.refs_2_), kind=kOutput, calls=%fused_computation.18 | convolution fusion | flops 10085990400 | bytes 34734080 | tf_op jit(solution)/shard_map/dot_general | solution.py:33
  302.7 53.1 %all-gather.8.cloned.1.call-done.refs_1_ = bf16[2560,1920]{1,0:T(8,128)(2,1)} async-done(((bf16[320,1920]{1,0:T(8,128)(2,1)}), bf16[2560,1920]{1,0:T(8,128)(2,1)}) %all-gather.8.cloned.1.call-update) | async-done | bytes 9830416 | tf_op jit(solution)/shard_map/all_gather | solution.py:509
  355.8 23.5 %fusion.53 = (bf16[1024,1920]{1,0:T(8,128)(2,1)}, f32[1024]{0:T(1024)S(1)}, bf16[1024,1920]{1,0:T(8,128)(2,1)}) fusion(f32[1024,1920]{1,0:T(8,128)} %fusion.4, f32[1024,1920]{1,0:T(8,128)} %get-tuple-element.58, bf16[1024,2560]{1,0:T(8,128)(2,1)} %left_ref.1, bf16[2560,1920]{1,0:T(8,128)(2,1)} %all-gather.8.cloned.1.call-done.refs_1_), kind=kOutput, calls=%fused_computation.150 | convolution fusion | flops 10117446656 | bytes 38670336 | tf_op jit(solution)/shard_map/dot_general | solution.py:33
  379.3 33.5 %shard_map.170 = (bf16[2,512,640]{2,1,0:T(8,128)(2,1)}, bf16[2,512,640]{2,1,0:T(8,128)(2,1)}, bf16[2,512,640]{2,1,0:T(8,128)(2,1)S(1)}, bf16[2,512,640]{2,1,0:T(8,128)(2,1)S(1)}) custom-call(s32[1]{0:T(128)} %bitcast.me_ref, bf16[1024,1920]{1,0:T(8,128)(2,1)} %get-tuple-element.99.refs_0_.right_ref, bf16[1024,1920]{1,0:T(8,128)(2,1)} %get-tuple-element.101.refs_1_.right_ref, ...), custom_call_target="tpu_custom_call" | custom-call | flops 20132659200 | bytes 32768000 | tf_op jit(solution)/shard_map/pallas_call | solution.py:410
  417.4 29.0 %collective-permute-done.20 = f32[8,128]{1,0:T(8,128)S(1)} collective-permute-done((f32[8,128]{1,0:T(8,128)S(1)}, f32[8,128]{1,0:T(8,128)S(1)}, u32[]{:S(2)}, u32[]{:S(2)}) %collective-permute-start.20) | collective-permute-done | bytes 4128 | tf_op jit(solution)/shard_map/ppermute | solution.py:38
  452.7 15.5 %shard_map.171 = (bf16[1280,1920]{1,0:T(8,128)(2,1)}, bf16[1280,1920]{1,0:T(8,128)(2,1)}) custom-call(s32[1]{0:T(128)} %bitcast.19.core_ref, bf16[1024,2560]{1,0:T(8,128)(2,1)} %fusion.1.left_ref, bf16[1024,1920]{1,0:T(8,128)(2,1)S(1)} %copy-done.23), custom_call_target="tpu_custom_call" | custom-call | flops 10066329600 | bytes 19005440 | tf_op jit(solution)/shard_map/pallas_call | solution.py:330
  471.6 4.0 fusion.54
  476.7 27.9 %collective-permute-done.26.along_x = bf16[1024,640]{1,0:T(8,128)(2,1)S(1)} collective-permute-done((bf16[1024,640]{1,0:T(8,128)(2,1)S(1)}, bf16[1024,640]{1,0:T(8,128)(2,1)S(1)}, u32[]{:S(2)}, u32[]{:S(2)}) %collective-permute-start.26) | collective-permute-done | bytes 1310752 | tf_op jit(solution)/shard_map/ppermute | solution.py:38
  505.3 2.1 collective-permute-start.29
  507.4 11.4 %collective-permute-done.28.top = bf16[512,640]{1,0:T(8,128)(2,1)S(1)} collective-permute-done((bf16[512,640]{1,0:T(8,128)(2,1)S(1)}, bf16[512,640]{1,0:T(8,128)(2,1)S(1)}, u32[]{:S(2)}, u32[]{:S(2)}) %collective-permute-start.28) | collective-permute-done | bytes 655392 | tf_op jit(solution)/shard_map/ppermute | solution.py:38
  519.2 6.6 shard_map.173
  525.8 7.6 shard_map.176
  533.4 3.7 collective-permute-done.46
  537.1 3.0 add_convert_fusion.4
  540.2 7.5 add_convert_fusion.1
  547.8 2.1 copy-done.22
  549.9 15.6 %shard_map.177 = (bf16[1280,1920]{1,0:T(8,128)(2,1)}, bf16[1280,1920]{1,0:T(8,128)(2,1)}) custom-call(s32[1]{0:T(128)} %bitcast.19.core_ref, bf16[1024,2560]{1,0:T(8,128)(2,1)} %fusion.1.left_ref, bf16[1024,1920]{1,0:T(8,128)(2,1)S(1)} %copy-done.22), custom_call_target="tpu_custom_call" | custom-call | flops 10066329600 | bytes 19005440 | tf_op jit(solution)/shard_map/pallas_call | solution.py:330
  565.5 8.4 collective-permute-done.47
  573.9 5.9 add_convert_fusion.2
  579.9 4.5 all-to-all-start.2
  584.5 17.0 %all-to-all-done.2 = bf16[4,256,640]{2,1,0:T(8,128)(2,1)} async-done(((bf16[4,256,640]{2,1,0:T(8,128)(2,1)}), bf16[4,256,640]{2,1,0:T(8,128)(2,1)}, u32[]{:S(2)}, u32[]{:S(2)}) %all-to-all-start.2) | async-done | bytes 1310752 | tf_op jit(solution)/shard_map/all_to_all | solution.py:142
  603.5 15.7 %attention_backward.1 = (bf16[256,2560]{1,0:T(8,128)(2,1)S(1)}, f32[1024,512]{1,0:T(8,128)S(1)}) custom-call(s32[1]{0:T(128)} %bitcast.1.first_ref, bf16[256,3072]{1,0:T(8,128)(2,1)S(1)} %bitcast.114, bf16[1024,512]{1,0:T(8,128)(2,1)S(1)} %copy-done.11, f32[256,128]{1,0:T(8,128)S(1)} %copy-done.17, f32[256,128]{1,0:T(8,128)S(1)} %copy-done.15, ...), custom_call_target="tpu_custom_call" | custom-call | flops 6710886400 | bytes 8388608 | tf_op jit(solution)/shard_map/attention_backward/pallas_call | solution.py:250
  621.8 5.3 collective-permute-done.30
  628.6 3.5 collective-permute-done.31
  633.7 3.5 collective-permute-done.33
  638.3 20.7 %all_to_all.77 = bf16[256,4,768]{2,0,1:T(8,128)(2,1)} all-to-all(bf16[256,4,768]{2,0,1:T(8,128)(2,1)S(1)} %bitcast.122), channel_id=1, replica_groups=mesh['tok'=8,'mdl'=4] {'mdl'}, dimensions={1} | all-to-all | bytes 3145728 | tf_op jit(solution)/shard_map/all_to_all | solution.py:146
  658.9 9.5 %shard_map.174 = (bf16[2,512,640]{2,1,0:T(8,128)(2,1)S(1)}, bf16[2,512,640]{2,1,0:T(8,128)(2,1)}, bf16[2,512,640]{2,1,0:T(8,128)(2,1)S(1)}, bf16[2,512,640]{2,1,0:T(8,128)(2,1)S(1)}) custom-call(s32[1]{0:T(128)} %bitcast.me_ref, bf16[1024,768]{1,0:T(8,128)(2,1)} %bitcast.120, bf16[2560,1408]{1,0:T(8,128)(2,1)} %all-gather.4.cloned.1.call-done.refs_1_.weight_ref.refs_0_), custom_call_target="tpu_custom_call" | custom-call | flops 4026531840 | bytes 14024704 | tf_op jit(solution)/shard_map/pallas_call | solution.py:410
  669.9 9.9 %shard_map.175 = (bf16[1280,768]{1,0:T(8,128)(2,1)S(1)}, bf16[1280,768]{1,0:T(8,128)(2,1)}, f32[2560,1]{1,0:T(8,128)S(1)}) custom-call(s32[1]{0:T(128)} %bitcast.19.core_ref, bf16[1024,2560]{1,0:T(8,128)(2,1)} %copy-done.34, bf16[1024,768]{1,0:T(8,128)(2,1)S(1)} %multiply_convert_fusion.1.right_ref, ...), custom_call_target="tpu_custom_call" | custom-call | flops 4026531840 | bytes 10747904 | tf_op jit(solution)/shard_map/pallas_call | solution.py:330
  679.8 15.5 %shard_map.178 = (bf16[1280,1920]{1,0:T(8,128)(2,1)}, bf16[1280,1920]{1,0:T(8,128)(2,1)}) custom-call(s32[1]{0:T(128)} %bitcast.19.core_ref, bf16[1024,2560]{1,0:T(8,128)(2,1)} %left_ref.1, bf16[1024,1920]{1,0:T(8,128)(2,1)S(1)} %copy-done.21), custom_call_target="tpu_custom_call" | custom-call | flops 10066329600 | bytes 19005440 | tf_op jit(solution)/shard_map/pallas_call | solution.py:330
  697.7 6.3 collective-permute-done.51
  703.9 7.5 add_convert_fusion
  711.4 17.2 %shard_map.172 = (bf16[2,512,640]{2,1,0:T(8,128)(2,1)S(1)}, bf16[2,512,640]{2,1,0:T(8,128)(2,1)S(1)}, bf16[2,512,640]{2,1,0:T(8,128)(2,1)S(1)}, bf16[2,512,640]{2,1,0:T(8,128)(2,1)S(1)}) custom-call(s32[1]{0:T(128)} %bitcast.me_ref, bf16[1024,1920]{1,0:T(8,128)(2,1)} %get-tuple-element.67.refs_0_.right_ref, ...), custom_call_target="tpu_custom_call" | custom-call | flops 10066329600 | bytes 19005440 | tf_op jit(solution)/shard_map/pallas_call | solution.py:410
  730.1 29.7 %collective-permute-done.24 = bf16[2,512,640]{2,1,0:T(8,128)(2,1)S(1)} collective-permute-done((bf16[2,512,640]{2,1,0:T(8,128)(2,1)S(1)}, bf16[2,512,640]{2,1,0:T(8,128)(2,1)S(1)}, u32[]{:S(2)}, u32[]{:S(2)}) %collective-permute-start.24) | collective-permute-done | bytes 1310752 | tf_op jit(solution)/shard_map/ppermute | solution.py:38
  768.5 10.3 %collective-permute-done.25 = bf16[512,640]{1,0:T(8,128)(2,1)} collective-permute-done((bf16[512,640]{1,0:T(8,128)(2,1)}, bf16[512,640]{1,0:T(8,128)(2,1)}, u32[]{:S(2)}, u32[]{:S(2)}) %collective-permute-start.25) | collective-permute-done | bytes 655392 | tf_op jit(solution)/shard_map/ppermute | solution.py:38
  778.9 2.8 bitcast_add_fusion.2
  787.2 19.0 %collective-permute-done.23 = bf16[512,640]{1,0:T(8,128)(2,1)S(1)} collective-permute-done((bf16[512,640]{1,0:T(8,128)(2,1)}, bf16[512,640]{1,0:T(8,128)(2,1)S(1)}, u32[]{:S(2)}, u32[]{:S(2)}) %collective-permute-start.23) | collective-permute-done | bytes 655392 | tf_op jit(solution)/shard_map/ppermute | solution.py:38
  806.1 2.6 bitcast_add_fusion.3
  813.8 2.1 fusion.27
  821.1 9.2 %collective-permute-done.37 = bf16[512,640]{1,0:T(8,128)(2,1)S(1)} collective-permute-done((bf16[512,640]{1,0:T(8,128)(2,1)}, bf16[512,640]{1,0:T(8,128)(2,1)S(1)}, u32[]{:S(2)}, u32[]{:S(2)}) %collective-permute-start.37) | collective-permute-done | bytes 655392 | tf_op jit(solution)/shard_map/ppermute | solution.py:38
  835.0 4.6 fusion.12
  841.7 5.2 convert_multiply_fusion.3
  847.7 2.1 convert_multiply_fusion.7
  851.0 39.5 %reduce-scatter.14.cloned.1.call-done = bf16[320,1920]{1,0:T(8,128)(2,1)} async-done(((bf16[1280,1920]{1,0:T(8,128)(2,1)}), bf16[320,1920]{1,0:T(8,128)(2,1)}) %reduce-scatter.14.cloned.1.call-update) | async-done | bytes 1228816 | tf_op jit(solution)/shard_map/reduce_scatter | solution.py:517
  890.5 2.9 convert_bitcast_fusion
  (327 shorter events, 106.8 us)
Async XLA Ops:
  7.2 79.2 %all-gather.4.cloned.1.call-start = ((), (), s32[]{:S(2)}) async-start(), calls=%async_computation.9 | async-start | bytes 8110080 | tf_op jit(solution)/shard_map/all_gather | solution.py:509
  11.3 254.2 %all-gather.6.cloned.1.call-start = ((), (), s32[]{:S(2)}) async-start(), calls=%async_computation.10 | async-start | bytes 22118400 | tf_op jit(solution)/shard_map/all_gather | solution.py:509
  13.6 342.2 %all-gather.8.cloned.1.call-start = ((), (), s32[]{:S(2)}) async-start(), calls=%async_computation.11 | async-start | bytes 11059200 | tf_op jit(solution)/shard_map/all_gather | solution.py:509
  14.9 31.7 %collective-permute-start = (bf16[1024,640]{1,0:T(8,128)(2,1)S(1)}, bf16[1024,640]{1,0:T(8,128)(2,1)S(1)}, u32[]{:S(2)}, u32[]{:S(2)}) collective-permute-start(bf16[1024,640]{1,0:T(8,128)(2,1)S(1)} %copy-done.30), channel_id=1, source_target_pairs={{0,1},{1,0},{2,3},{3,2},{4,5},{5,4},{6,7},{7,6},{8,9},{9,8},{10,11... | collective-permute-start | bytes 3932168 | tf_op jit(solution)/shard_map/ppermute | solution.py:38
  17.9 31.4 %collective-permute-start.1 = (bf16[1024,640]{1,0:T(8,128)(2,1)S(1)}, bf16[1024,640]{1,0:T(8,128)(2,1)S(1)}, u32[]{:S(2)}, u32[]{:S(2)}) collective-permute-start(bf16[1024,640]{1,0:T(8,128)(2,1)S(1)} %copy-done.30), channel_id=1, source_target_pairs={{0,2},{1,3},{2,0},{3,1},{4,6},{5,7},{6,4},{7,5},{8,10},{9,11},{10,... | collective-permute-start | bytes 3932168 | tf_op jit(solution)/shard_map/ppermute | solution.py:38
  47.5 16.2 %collective-permute-start.2 = (bf16[512,640]{1,0:T(8,128)(2,1)}, bf16[512,640]{1,0:T(8,128)(2,1)S(1)}, u32[]{:S(2)}, u32[]{:S(2)}) collective-permute-start(bf16[512,640]{1,0:T(8,128)(2,1)} %slice.220), channel_id=1, source_target_pairs={{0,2},{1,3},{2,0},{3,1},{4,6},{5,7},{6,4},{7,5},{8,10},{9,11},{10,... | collective-permute-start | bytes 1966088 | tf_op jit(solution)/shard_map/ppermute | solution.py:38
  51.3 15.8 %collective-permute-start.3 = (bf16[512,640]{1,0:T(8,128)(2,1)}, bf16[512,640]{1,0:T(8,128)(2,1)}, u32[]{:S(2)}, u32[]{:S(2)}) collective-permute-start(bf16[512,640]{1,0:T(8,128)(2,1)} %slice.221), channel_id=1, source_target_pairs={{0,1},{1,0},{2,3},{3,2},{4,5},{5,4},{6,7},{7,6},{8,9},{9,8},{10,11... | collective-permute-start | bytes 1966088 | tf_op jit(solution)/shard_map/ppermute | solution.py:38
  95.5 23.6 %all-to-all-start = ((bf16[4,256,768]{2,1,0:T(8,128)(2,1)}), bf16[4,256,768]{2,1,0:T(8,128)(2,1)S(1)}, u32[]{:S(2)}, u32[]{:S(2)}) async-start(bf16[4,256,768]{2,1,0:T(8,128)(2,1)} %bitcast.3), calls=%async_computation | async-start | bytes 3145728 | tf_op jit(solution)/shard_map/all_to_all | solution.py:142
  99.3 740.4 %reduce-scatter.8.cloned.1.call-start = ((), (), s32[]{:S(2)}) async-start(), calls=%async_computation.13 | async-start | bytes 2048000 | tf_op jit(solution)/shard_map/reduce_scatter | solution.py:517
  121.7 7.8 collective-permute-start.4
  123.1 8.0 collective-permute-start.5
  129.6 5.0 collective-permute-start.6
  131.1 5.0 collective-permute-start.7
  173.4 27.2 %collective-permute-start.10 = (bf16[2,512,640]{2,1,0:T(8,128)(2,1)S(1)}, bf16[2,512,640]{2,1,0:T(8,128)(2,1)S(1)}, u32[]{:S(2)}, u32[]{:S(2)}) collective-permute-start(bf16[2,512,640]{2,1,0:T(8,128)(2,1)S(1)} %get-tuple-element.56), channel_id=1, source_target_pairs={{0,2},{1,3},{2,0},{3,1},{4,6},{5,7},{6,4},{7,5},{8,10},{9,11},{10,... | collective-permute-start | bytes 3932168 | tf_op jit(solution)/shard_map/ppermute | solution.py:38
  174.5 29.6 %collective-permute-start.8 = (bf16[2,512,640]{2,1,0:T(8,128)(2,1)S(1)}, bf16[2,512,640]{2,1,0:T(8,128)(2,1)S(1)}, u32[]{:S(2)}, u32[]{:S(2)}) collective-permute-start(bf16[2,512,640]{2,1,0:T(8,128)(2,1)S(1)} %get-tuple-element.54), channel_id=1, source_target_pairs={{0,1},{1,0},{2,3},{3,2},{4,5},{5,4},{6,7},{7,6},{8,9},{9,8},{10,11... | collective-permute-start | bytes 3932168 | tf_op jit(solution)/shard_map/ppermute | solution.py:38
  200.8 14.8 %collective-permute-start.11 = (bf16[512,640]{1,0:T(8,128)(2,1)S(1)}, bf16[512,640]{1,0:T(8,128)(2,1)S(1)}, u32[]{:S(2)}, u32[]{:S(2)}) collective-permute-start(bf16[512,640]{1,0:T(8,128)(2,1)S(1)} %fusion.21), channel_id=1, source_target_pairs={{0,1},{1,0},{2,3},{3,2},{4,5},{5,4},{6,7},{7,6},{8,9},{9,8},{10,11... | collective-permute-start | bytes 1966088 | tf_op jit(solution)/shard_map/ppermute | solution.py:38
  204.2 11.6 %collective-permute-start.9 = (bf16[512,640]{1,0:T(8,128)(2,1)S(1)}, bf16[512,640]{1,0:T(8,128)(2,1)S(1)}, u32[]{:S(2)}, u32[]{:S(2)}) collective-permute-start(bf16[512,640]{1,0:T(8,128)(2,1)S(1)} %fusion.20), channel_id=1, source_target_pairs={{0,2},{1,3},{2,0},{3,1},{4,6},{5,7},{6,4},{7,5},{8,10},{9,11},{10,... | collective-permute-start | bytes 1966088 | tf_op jit(solution)/shard_map/ppermute | solution.py:38
  218.5 28.2 %collective-permute-start.12 = (bf16[1024,640]{1,0:T(8,128)(2,1)S(1)}, bf16[1024,640]{1,0:T(8,128)(2,1)S(1)}, u32[]{:S(2)}, u32[]{:S(2)}) collective-permute-start(bf16[1024,640]{1,0:T(8,128)(2,1)S(1)} %get-tuple-element.98), channel_id=1, source_target_pairs={{0,1},{1,0},{2,3},{3,2},{4,5},{5,4},{6,7},{7,6},{8,9},{9,8},{10,11... | collective-permute-start | bytes 3932168 | tf_op jit(solution)/shard_map/ppermute | solution.py:38
  219.2 29.3 %collective-permute-start.13 = (bf16[1024,640]{1,0:T(8,128)(2,1)S(1)}, bf16[1024,640]{1,0:T(8,128)(2,1)S(1)}, u32[]{:S(2)}, u32[]{:S(2)}) collective-permute-start(bf16[1024,640]{1,0:T(8,128)(2,1)S(1)} %get-tuple-element.98), channel_id=1, source_target_pairs={{0,2},{1,3},{2,0},{3,1},{4,6},{5,7},{6,4},{7,5},{8,10},{9,11},{10,... | collective-permute-start | bytes 3932168 | tf_op jit(solution)/shard_map/ppermute | solution.py:38
  246.8 14.1 %collective-permute-start.14 = (bf16[512,640]{1,0:T(8,128)(2,1)S(1)}, bf16[512,640]{1,0:T(8,128)(2,1)S(1)}, u32[]{:S(2)}, u32[]{:S(2)}) collective-permute-start(bf16[512,640]{1,0:T(8,128)(2,1)S(1)} %slice.233), channel_id=1, source_target_pairs={{0,2},{1,3},{2,0},{3,1},{4,6},{5,7},{6,4},{7,5},{8,10},{9,11},{10,... | collective-permute-start | bytes 1966088 | tf_op jit(solution)/shard_map/ppermute | solution.py:38
  248.5 12.5 %collective-permute-start.15 = (bf16[512,640]{1,0:T(8,128)(2,1)S(1)}, bf16[512,640]{1,0:T(8,128)(2,1)S(1)}, u32[]{:S(2)}, u32[]{:S(2)}) collective-permute-start(bf16[512,640]{1,0:T(8,128)(2,1)S(1)} %slice.234), channel_id=1, source_target_pairs={{0,1},{1,0},{2,3},{3,2},{4,5},{5,4},{6,7},{7,6},{8,9},{9,8},{10,11... | collective-permute-start | bytes 1966088 | tf_op jit(solution)/shard_map/ppermute | solution.py:38
  413.9 33.0 %collective-permute-start.18 = (bf16[2,512,640]{2,1,0:T(8,128)(2,1)}, bf16[2,512,640]{2,1,0:T(8,128)(2,1)}, u32[]{:S(2)}, u32[]{:S(2)}) collective-permute-start(bf16[2,512,640]{2,1,0:T(8,128)(2,1)} %get-tuple-element.63), channel_id=1, source_target_pairs={{0,2},{1,3},{2,0},{3,1},{4,6},{5,7},{6,4},{7,5},{8,10},{9,11},{10,... | collective-permute-start | bytes 3932168 | tf_op jit(solution)/shard_map/ppermute | solution.py:38
  415.3 34.6 %collective-permute-start.16 = (bf16[2,512,640]{2,1,0:T(8,128)(2,1)}, bf16[2,512,640]{2,1,0:T(8,128)(2,1)}, u32[]{:S(2)}, u32[]{:S(2)}) collective-permute-start(bf16[2,512,640]{2,1,0:T(8,128)(2,1)} %get-tuple-element.61), channel_id=1, source_target_pairs={{0,1},{1,0},{2,3},{3,2},{4,5},{5,4},{6,7},{7,6},{8,9},{9,8},{10,11... | collective-permute-start | bytes 3932168 | tf_op jit(solution)/shard_map/ppermute | solution.py:38
  416.8 29.5 %collective-permute-start.20 = (f32[8,128]{1,0:T(8,128)S(1)}, f32[8,128]{1,0:T(8,128)S(1)}, u32[]{:S(2)}, u32[]{:S(2)}) collective-permute-start(f32[8,128]{1,0:T(8,128)S(1)} %bitcast.129), channel_id=1, source_target_pairs={{0,1},{1,0},{2,3},{3,2},{4,5},{5,4},{6,7},{7,6},{8,9},{9,8},{10,11... | collective-permute-start | bytes 12296 | tf_op jit(solution)/shard_map/ppermute | solution.py:38
  446.3 21.8 %collective-permute-start.21 = (f32[8,128]{1,0:T(8,128)S(1)}, f32[8,128]{1,0:T(8,128)S(1)}, u32[]{:S(2)}, u32[]{:S(2)}) collective-permute-start(f32[8,128]{1,0:T(8,128)S(1)} %bitcast_add_fusion.8), channel_id=1, source_target_pairs={{0,2},{1,3},{2,0},{3,1},{4,6},{5,7},{6,4},{7,5},{8,10},{9,11},{10,... | collective-permute-start | bytes 12296 | tf_op jit(solution)/shard_map/ppermute | solution.py:38
  448.3 19.8 %collective-permute-start.19 = (bf16[512,640]{1,0:T(8,128)(2,1)S(1)}, bf16[512,640]{1,0:T(8,128)(2,1)S(1)}, u32[]{:S(2)}, u32[]{:S(2)}) collective-permute-start(bf16[512,640]{1,0:T(8,128)(2,1)S(1)} %fusion.23), channel_id=1, source_target_pairs={{0,1},{1,0},{2,3},{3,2},{4,5},{5,4},{6,7},{7,6},{8,9},{9,8},{10,11... | collective-permute-start | bytes 1966088 | tf_op jit(solution)/shard_map/ppermute | solution.py:38
  451.1 18.6 %collective-permute-start.17 = (bf16[512,640]{1,0:T(8,128)(2,1)S(1)}, bf16[512,640]{1,0:T(8,128)(2,1)S(1)}, u32[]{:S(2)}, u32[]{:S(2)}) collective-permute-start(bf16[512,640]{1,0:T(8,128)(2,1)S(1)} %fusion.22), channel_id=1, source_target_pairs={{0,2},{1,3},{2,0},{3,1},{4,6},{5,7},{6,4},{7,5},{8,10},{9,11},{10,... | collective-permute-start | bytes 1966088 | tf_op jit(solution)/shard_map/ppermute | solution.py:38
  469.7 49.5 %slice-start = ((s8[7208960]{0:T(1024)(128)(4,1)}), s8[4194304]{0:T(1024)(128)(4,1)S(1)}, s32[]{:S(2)}) async-start(s8[7208960]{0:T(1024)(128)(4,1)} %bitcast.110), calls=%async_computation.17 | async-start | bytes 8388608
  471.6 47.6 %slice-start.1 = ((s8[7208960]{0:T(1024)(128)(4,1)}), s8[3014656]{0:T(1024)(128)(4,1)S(1)}, s32[]{:S(2)}) async-start(s8[7208960]{0:T(1024)(128)(4,1)} %bitcast.110), calls=%async_computation.18 | async-start | bytes 6029312
  475.6 29.0 %collective-permute-start.26 = (bf16[1024,640]{1,0:T(8,128)(2,1)S(1)}, bf16[1024,640]{1,0:T(8,128)(2,1)S(1)}, u32[]{:S(2)}, u32[]{:S(2)}) collective-permute-start(bf16[1024,640]{1,0:T(8,128)(2,1)S(1)} %get-tuple-element.66.own), channel_id=1, source_target_pairs={{0,1},{1,0},{2,3},{3,2},{4,5},{5,4},{6,7},{7,6},{8,9},{9,8},{10,11... | collective-permute-start | bytes 3932168 | tf_op jit(solution)/shard_map/ppermute | solution.py:38
  476.2 29.1 %collective-permute-start.27 = (bf16[1024,640]{1,0:T(8,128)(2,1)S(1)}, bf16[1024,640]{1,0:T(8,128)(2,1)S(1)}, u32[]{:S(2)}, u32[]{:S(2)}) collective-permute-start(bf16[1024,640]{1,0:T(8,128)(2,1)S(1)} %get-tuple-element.66.own), channel_id=1, source_target_pairs={{0,2},{1,3},{2,0},{3,1},{4,6},{5,7},{6,4},{7,5},{8,10},{9,11},{10,... | collective-permute-start | bytes 3932168 | tf_op jit(solution)/shard_map/ppermute | solution.py:38
  504.6 14.3 %collective-permute-start.28 = (bf16[512,640]{1,0:T(8,128)(2,1)S(1)}, bf16[512,640]{1,0:T(8,128)(2,1)S(1)}, u32[]{:S(2)}, u32[]{:S(2)}) collective-permute-start(bf16[512,640]{1,0:T(8,128)(2,1)S(1)} %slice.245), channel_id=1, source_target_pairs={{0,2},{1,3},{2,0},{3,1},{4,6},{5,7},{6,4},{7,5},{8,10},{9,11},{10,... | collective-permute-start | bytes 1966088 | tf_op jit(solution)/shard_map/ppermute | solution.py:38
  505.3 13.9 %collective-permute-start.29 = (bf16[512,640]{1,0:T(8,128)(2,1)S(1)}, bf16[512,640]{1,0:T(8,128)(2,1)S(1)}, u32[]{:S(2)}, u32[]{:S(2)}) collective-permute-start(bf16[512,640]{1,0:T(8,128)(2,1)S(1)} %slice.246), channel_id=1, source_target_pairs={{0,1},{1,0},{2,3},{3,2},{4,5},{5,4},{6,7},{7,6},{8,9},{9,8},{10,11... | collective-permute-start | bytes 1966088 | tf_op jit(solution)/shard_map/ppermute | solution.py:38
  507.4 32.8 %collective-permute-start.48 = (bf16[1280,1920]{1,0:T(8,128)(2,1)}, bf16[1280,1920]{1,0:T(8,128)(2,1)}, u32[]{:S(2)}, u32[]{:S(2)}) collective-permute-start(bf16[1280,1920]{1,0:T(8,128)(2,1)} %get-tuple-element.91), channel_id=1, source_target_pairs={{0,4},{4,0},{8,12},{12,8},{16,20},{20,16},{24,28},{28,24},{1,5},{5... | collective-permute-start | bytes 14745608 | tf_op jit(solution)/shard_map/ppermute | solution.py:514
  533.4 3.7 collective-permute-start.46
  540.2 301.5 %reduce-scatter.12.cloned.1.call-start = ((), (), s32[]{:S(2)}) async-start(), calls=%async_computation.15 | async-start | bytes 6144000 | tf_op jit(solution)/shard_map/reduce_scatter | solution.py:517
  547.7 293.9 %reduce-scatter.10.cloned.1.call-start = ((), (), s32[]{:S(2)}) async-start(), calls=%async_computation.14 | async-start | bytes 6144000 | tf_op jit(solution)/shard_map/reduce_scatter | solution.py:517
  565.5 8.4 collective-permute-start.47
  579.9 21.6 %all-to-all-start.2 = ((bf16[4,256,640]{2,1,0:T(8,128)(2,1)}), bf16[4,256,640]{2,1,0:T(8,128)(2,1)}, u32[]{:S(2)}, u32[]{:S(2)}) async-start(bf16[4,256,640]{2,1,0:T(8,128)(2,1)} %bitcast.24), calls=%async_computation.2 | async-start | bytes 2621440 | tf_op jit(solution)/shard_map/all_to_all | solution.py:142
  584.4 263.3 %reduce-scatter.6.cloned.1.call-start = ((), (), s32[]{:S(2)}) async-start(), calls=%async_computation.12 | async-start | bytes 2457600 | tf_op jit(solution)/shard_map/reduce_scatter | solution.py:517
  619.5 7.6 collective-permute-start.30
  621.0 7.6 collective-permute-start.32
  627.1 5.0 collective-permute-start.31
  632.2 5.0 collective-permute-start.33
  679.8 16.0 %collective-permute-start.45 = (bf16[1280,768]{1,0:T(8,128)(2,1)}, bf16[1280,768]{1,0:T(8,128)(2,1)S(1)}, u32[]{:S(2)}, u32[]{:S(2)}) collective-permute-start(bf16[1280,768]{1,0:T(8,128)(2,1)} %get-tuple-element.83), channel_id=1, source_target_pairs={{0,4},{4,0},{8,12},{12,8},{16,20},{20,16},{24,28},{28,24},{1,5},{5... | collective-permute-start | bytes 5898248 | tf_op jit(solution)/shard_map/ppermute | solution.py:514
  695.3 8.6 collective-permute-start.51
  697.6 192.9 %reduce-scatter.14.cloned.1.call-start = ((), (), s32[]{:S(2)}) async-start(), calls=%async_computation.16 | async-start | bytes 6144000 | tf_op jit(solution)/shard_map/reduce_scatter | solution.py:517
  728.6 31.1 %collective-permute-start.24 = (bf16[2,512,640]{2,1,0:T(8,128)(2,1)S(1)}, bf16[2,512,640]{2,1,0:T(8,128)(2,1)S(1)}, u32[]{:S(2)}, u32[]{:S(2)}) collective-permute-start(bf16[2,512,640]{2,1,0:T(8,128)(2,1)S(1)} %get-tuple-element.71), channel_id=1, source_target_pairs={{0,2},{1,3},{2,0},{3,1},{4,6},{5,7},{6,4},{7,5},{8,10},{9,11},{10,... | collective-permute-start | bytes 3932168 | tf_op jit(solution)/shard_map/ppermute | solution.py:38
  729.3 33.1 %collective-permute-start.22 = (bf16[2,512,640]{2,1,0:T(8,128)(2,1)S(1)}, bf16[2,512,640]{2,1,0:T(8,128)(2,1)S(1)}, u32[]{:S(2)}, u32[]{:S(2)}) collective-permute-start(bf16[2,512,640]{2,1,0:T(8,128)(2,1)S(1)} %get-tuple-element.69), channel_id=1, source_target_pairs={{0,1},{1,0},{2,3},{3,2},{4,5},{5,4},{6,7},{7,6},{8,9},{9,8},{10,11... | collective-permute-start | bytes 3932168 | tf_op jit(solution)/shard_map/ppermute | solution.py:38
  760.9 17.9 %collective-permute-start.25 = (bf16[512,640]{1,0:T(8,128)(2,1)}, bf16[512,640]{1,0:T(8,128)(2,1)}, u32[]{:S(2)}, u32[]{:S(2)}) collective-permute-start(bf16[512,640]{1,0:T(8,128)(2,1)} %fusion.25), channel_id=1, source_target_pairs={{0,1},{1,0},{2,3},{3,2},{4,5},{5,4},{6,7},{7,6},{8,9},{9,8},{10,11... | collective-permute-start | bytes 1966088 | tf_op jit(solution)/shard_map/ppermute | solution.py:38
  761.8 52.0 %collective-permute-start.36 = (bf16[2,512,640]{2,1,0:T(8,128)(2,1)}, bf16[2,512,640]{2,1,0:T(8,128)(2,1)}, u32[]{:S(2)}, u32[]{:S(2)}) collective-permute-start(bf16[2,512,640]{2,1,0:T(8,128)(2,1)} %get-tuple-element.78), channel_id=1, source_target_pairs={{0,2},{1,3},{2,0},{3,1},{4,6},{5,7},{6,4},{7,5},{8,10},{9,11},{10,... | collective-permute-start | bytes 3932168 | tf_op jit(solution)/shard_map/ppermute | solution.py:38
  763.6 42.5 %collective-permute-start.23 = (bf16[512,640]{1,0:T(8,128)(2,1)}, bf16[512,640]{1,0:T(8,128)(2,1)S(1)}, u32[]{:S(2)}, u32[]{:S(2)}) collective-permute-start(bf16[512,640]{1,0:T(8,128)(2,1)} %fusion.24), channel_id=1, source_target_pairs={{0,2},{1,3},{2,0},{3,1},{4,6},{5,7},{6,4},{7,5},{8,10},{9,11},{10,... | collective-permute-start | bytes 1966088 | tf_op jit(solution)/shard_map/ppermute | solution.py:38
  766.3 50.6 %collective-permute-start.34 = (bf16[2,512,640]{2,1,0:T(8,128)(2,1)}, bf16[2,512,640]{2,1,0:T(8,128)(2,1)}, u32[]{:S(2)}, u32[]{:S(2)}) collective-permute-start(bf16[2,512,640]{2,1,0:T(8,128)(2,1)} %copy-done.18), channel_id=1, source_target_pairs={{0,1},{1,0},{2,3},{3,2},{4,5},{5,4},{6,7},{7,6},{8,9},{9,8},{10,11... | collective-permute-start | bytes 3932168 | tf_op jit(solution)/shard_map/ppermute | solution.py:38
  768.5 13.1 %collective-permute-start.40 = (f32[8,320]{1,0:T(8,128)}, f32[8,320]{1,0:T(8,128)S(1)}, u32[]{:S(2)}, u32[]{:S(2)}) collective-permute-start(f32[8,320]{1,0:T(8,128)} %reshape.172), channel_id=1, source_target_pairs={{0,4},{4,0},{8,12},{12,8},{16,20},{20,16},{24,28},{28,24},{1,5},{5... | collective-permute-start | bytes 30728 | tf_op jit(solution)/shard_map/ppermute | solution.py:136
  781.7 4.6 collective-permute-start.41
  783.9 25.8 %collective-permute-start.38 = (f32[4,256]{1,0:T(4,128)S(1)}, f32[4,256]{1,0:T(4,128)}, u32[]{:S(2)}, u32[]{:S(2)}) collective-permute-start(f32[4,256]{1,0:T(4,128)S(1)} %dynamic_update_slice.65), channel_id=1, source_target_pairs={{0,1},{1,0},{2,3},{3,2},{4,5},{5,4},{6,7},{7,6},{8,9},{9,8},{10,11... | collective-permute-start | bytes 12296 | tf_op jit(solution)/shard_map/ppermute | solution.py:38
  787.0 21.7 %collective-permute-start.42 = (f32[8,320]{1,0:T(8,128)S(1)}, f32[8,320]{1,0:T(8,128)S(1)}, u32[]{:S(2)}, u32[]{:S(2)}) collective-permute-start(f32[8,320]{1,0:T(8,128)S(1)} %add.398), channel_id=1, source_target_pairs={{0,16},{4,20},{8,24},{12,28},{16,0},{20,4},{24,8},{28,12},{1,17},{... | collective-permute-start | bytes 30728 | tf_op jit(solution)/shard_map/ppermute | solution.py:136
  808.7 4.1 collective-permute-start.43
  811.7 7.9 collective-permute-start.39
  812.8 7.6 collective-permute-start.44
  815.8 14.5 %collective-permute-start.37 = (bf16[512,640]{1,0:T(8,128)(2,1)}, bf16[512,640]{1,0:T(8,128)(2,1)S(1)}, u32[]{:S(2)}, u32[]{:S(2)}) collective-permute-start(bf16[512,640]{1,0:T(8,128)(2,1)} %fusion.27), channel_id=1, source_target_pairs={{0,1},{1,0},{2,3},{3,2},{4,5},{5,4},{6,7},{7,6},{8,9},{9,8},{10,11... | collective-permute-start | bytes 1966088 | tf_op jit(solution)/shard_map/ppermute | solution.py:38
  819.0 14.5 %collective-permute-start.35 = (bf16[512,640]{1,0:T(8,128)(2,1)}, bf16[512,640]{1,0:T(8,128)(2,1)}, u32[]{:S(2)}, u32[]{:S(2)}) collective-permute-start(bf16[512,640]{1,0:T(8,128)(2,1)} %fusion.26), channel_id=1, source_target_pairs={{0,2},{1,3},{2,0},{3,1},{4,6},{5,7},{6,4},{7,5},{8,10},{9,11},{10,... | collective-permute-start | bytes 1966088 | tf_op jit(solution)/shard_map/ppermute | solution.py:38
  846.9 3.6 collective-permute-start.49
  850.5 42.9 %collective-permute-start.50 = (f32[320]{0:T(512)S(1)}, f32[320]{0:T(512)S(1)}, u32[]{:S(2)}, u32[]{:S(2)}) collective-permute-start(f32[320]{0:T(512)S(1)} %add.408), channel_id=1, source_target_pairs={{0,2},{1,3},{2,0},{3,1},{4,6},{5,7},{6,4},{7,5},{8,10},{9,11},{10,... | collective-permute-start | bytes 3848 | tf_op jit(solution)/shard_map/ppermute | solution.py:38
  (65 other events, 809.9 us)
Sparse Core Ops, SparseCore 0:
  11.4 74.9 all-gather.3
  88.7 173.2 all-gather.5
  263.6 92.1 all-gather.7
  540.3 33.8 reduce-scatter.7
  576.4 87.3 reduce-scatter.11
  666.0 88.9 reduce-scatter.9
  757.9 42.6 reduce-scatter.5
  802.9 87.5 reduce-scatter.13

commit v6 on v5

--- a/solution.py
+++ b/solution.py
@@ -338,6 +338,42 @@
     )(*operands)
 
 
+def part_kernel(core_ref, rows_ref, above_ref, d_gate_ref, d_up_ref, hidden_ref, kept, sent):
+    cols = hidden_ref.shape[1]
+    for at, (left_ref, right_ref) in enumerate(
+        ((rows_ref, d_gate_ref), (rows_ref, d_up_ref), (above_ref, hidden_ref))
+    ):
+        total = tn(left_ref[...], right_ref[...]).astype(BF16)
+        window = (slice(None), pl.ds(at * cols, cols))
+        keep_half(core_ref, total, kept.at[window], sent.at[window])
+
+
+def part_grad(rows, above, d_gate, d_up, hidden):
+    tokens, features = rows.shape
+    cols = hidden.shape[1]
+    pairs = lax.axis_size("tok") // 2
+    step = features // pairs
+    if step % 128 or cols % 128:
+        total = [tn(rows, d_gate), tn(rows, d_up), tn(above, hidden)]
+        total = jnp.concatenate(total, axis=1).astype(BF16)
+        return split_pairs(total, pairs, lax.axis_index("tok") % 2)
+    out = jax.ShapeDtypeStruct((features // 2, 3 * cols), BF16)
+    left_spec = pl.BlockSpec((tokens, step), lambda pair: (0, pair))
+    right_spec = pl.BlockSpec((tokens, cols), lambda pair: (0, 0))
+    return pl.pallas_call(
+        part_kernel,
+        grid=(pairs,),
+        out_shape=(out, out),
+        in_specs=[pl.BlockSpec(memory_space=pltpu.SMEM)] + [left_spec] * 2 + [right_spec] * 3,
+        out_specs=[pl.BlockSpec((step // 2, 3 * cols), lambda pair: (pair, 0))] * 2,
+        compiler_params=in_order(48),
+        cost_estimate=cost(
+            6 * tokens * features * cols,
+            2 * (2 * tokens * features + 3 * cols * (tokens + features)),
+        ),
+    )(core_index(), rows, above, d_gate, d_up, hidden)
+
+
 def pieces_grad_kernel(me_ref, core_ref, own, along_x, along_y, top, bottom, right_ref, kept, sent):
     at = pl.program_id(0)
     half = top.shape[0]
@@ -378,10 +414,40 @@
     )(me, core_index(), *pieces, right)
 
 
+def sum_kernel(starts, *refs):
+    *lefts, weight_ref, out_ref = refs
+    total = 0.0
+    for left_ref, start in zip(lefts, starts):
+        total += nt(left_ref[...], weight_ref[:, start : start + left_ref.shape[1]])
+    out_ref[...] = total
+
+
+def sum_products(lefts, weight, starts):
+    tokens = lefts[0].shape[0]
+    rows, cols = weight.shape
+    if lefts[0].shape[1] % 128:
+        return sum(
+            nt(left, weight[:, start : start + left.shape[1]])
+            for left, start in zip(lefts, starts)
+        )
+    step = 512
+    depth = sum(left.shape[1] for left in lefts)
+    return pl.pallas_call(
+        functools.partial(sum_kernel, starts),
+        grid=(rows // step,),
+        out_shape=jax.ShapeDtypeStruct((tokens, rows), F32),
+        in_specs=[pl.BlockSpec(left.shape, lambda row: (0, 0)) for left in lefts]
+        + [pl.BlockSpec((step, cols), lambda row: (row, 0))],
+        out_specs=pl.BlockSpec((tokens, step), lambda row: (0, row)),
+        compiler_params=in_order(48),
+        cost_estimate=cost(2 * tokens * rows * depth, 2 * rows * cols + 4 * tokens * rows),
+    )(*lefts, weight)
+
+
 def payload_kernel(starts, me_ref, *refs):
     lefts, weight_ref = refs[: len(starts)], refs[len(starts)]
-    top_sent, bottom_sent, top_kept, bottom_kept = refs[len(starts) + 1 :]
-    total = 0.0
+    top_sent, bottom_sent, top_kept, bottom_kept = refs[-4:]
+    total = refs[-5][...] if len(refs) == len(starts) + 6 else 0.0
     for left_ref, start in zip(lefts, starts):
         total += nt(left_ref[...], weight_ref[:, start : start + left_ref.shape[1]])
     total = total.astype(BF16)
@@ -400,7 +466,7 @@
             bottom[bottom_at] = total[half:]
 
 
-def scatter_product(lefts, weight, starts):
+def scatter_product(lefts, weight, starts, partial=()):
     tokens = lefts[0].shape[0]
     rows, cols = weight.shape
     step = rows // 4
@@ -413,13 +479,15 @@
             num_scalar_prefetch=1,
             grid=(4,),
             in_specs=[pl.BlockSpec(left.shape, lambda at, me_ref: (0, 0)) for left in lefts]
-            + [pl.BlockSpec((step, cols), lambda at, me_ref: (me_ref[0] ^ (3 - at), 0))],
+            + [pl.BlockSpec((step, cols), lambda at, me_ref: (me_ref[0] ^ (3 - at), 0))]
+            + [pl.BlockSpec((tokens, step), lambda at, me_ref: (0, me_ref[0] ^ (3 - at)))]
+            * len(partial),
             out_specs=[pl.BlockSpec(out.shape, lambda at, me_ref: (0, 0, 0))] * 4,
         ),
         out_shape=(out,) * 4,
         compiler_params=in_order(48),
         cost_estimate=cost(2 * tokens * rows * depth, 2 * (tokens * depth + rows * cols + tokens * rows)),
-    )(me, *lefts, weight)
+    )(me, *lefts, weight, *partial)
 
 
 def pieces_kernel(start, me_ref, own, along_x, along_y, top, bottom, weight_ref, out_ref, total):
@@ -463,13 +531,11 @@
     )(me, *pieces, weight)
 
 
-def product_to_mdl(lefts, weight, starts):
+def product_to_mdl(lefts, weight, starts, partial=()):
     if lax.axis_size("mdl") == 4:
-        payload = scatter_product(lefts, weight, starts)
+        payload = scatter_product(lefts, weight, starts, partial)
         return payload, lambda payload: scatter_payload(payload)
-    part = sum(
-        nt(left, weight[:, start : start + left.shape[1]]) for left, start in zip(lefts, starts)
-    )
+    part = sum((sum_products(lefts, weight, starts), *partial))
     return (part.astype(BF16),), lambda payload: scatter_mdl(payload[0], 1)
 
 
@@ -523,9 +589,13 @@
     attn_local = jnp.concatenate([scaled(qkv_weight, norm1_gain), out_weight.T], axis=1)
     w_attn = from_tok(attn_local, 0)
     w_qkv = w_attn[:, :qkv_cols]
-    gu_local = jnp.concatenate([scaled(w, norm2_gain) for w in (gate_weight, up_weight)], 1)
-    w_gu = from_tok(gu_local, 0)
-    w_down_t = from_tok(down_weight.T, 0)
+    middle = -(-ff_cols // 256) * 128
+    parts = ((0, middle), (middle, ff_cols))
+    w_parts = []
+    for start, stop in parts:
+        local = [scaled(w[:, start:stop], norm2_gain) for w in (gate_weight, up_weight)]
+        local = jnp.concatenate([*local, down_weight[start:stop].T], axis=1)
+        w_parts.append(from_tok(local, 0))
 
     rows_in = gather_mdl(inputs, 1)
     scale_one = row_scale(rows_in)
@@ -549,35 +619,42 @@
     rows_two = gather_mdl(mixed.astype(BF16), 1)
     scale_two = row_scale(rows_two)
     rows_hat = (rows_two.astype(F32) * scale_two).astype(BF16)
-    gate_in = nn(rows_hat, w_gu[:, :ff_cols])
-    up_in = nn(rows_hat, w_gu[:, ff_cols:])
-    gelu, _ = gelu_parts(gate_in)
-    hidden = (gelu * up_in).astype(BF16)
-    gate_in, up_in, hidden = lax.optimization_barrier((gate_in, up_in, hidden))
-    gelu, slope = gelu_parts(gate_in)
-
-    down_local = pair_grad(cotangent, hidden)
-    down_grad = pair_to_tok(down_local)
-    d_hidden = nn(cotangent, w_down_t)
-    d_gate_f = d_hidden * up_in * slope
-    d_up_f = d_hidden * gelu
-    stat_two = jnp.sum(d_gate_f * gate_in + d_up_f * up_in, axis=1)
-    d_gate, d_up = d_gate_f.astype(BF16), d_up_f.astype(BF16)
-    gate_local = pair_grad(rows_hat, d_gate)
-    gate_sum = pair_to_tok(gate_local)
-    payload, scatter = product_to_mdl((d_gate, d_up), w_gu, (0, ff_cols))
-    rows_later = after(rows_hat, payload[0])
-    up_local = pair_grad(rows_later, d_up)
-    up_sum = pair_to_tok(up_local)
+    rows, above, stat_two, partial, hiddens, sums = rows_hat, cotangent, 0.0, (), [], []
+    for index, (weight, (start, stop)) in enumerate(zip(w_parts, parts)):
+        cols = stop - start
+        last = index == len(parts) - 1
+        gate_in = nn(rows, weight[:, :cols])
+        up_in = nn(rows, weight[:, cols : 2 * cols])
+        d_hidden = nn(above, weight[:, 2 * cols :])
+        gelu, slope = gelu_parts(gate_in)
+        hidden = (gelu * up_in).astype(BF16)
+        d_gate = d_hidden * up_in * slope
+        d_up = d_hidden * gelu
+        stat_two += jnp.sum(d_gate * gate_in + d_up * up_in, axis=1)
+        d_gate, d_up = d_gate.astype(BF16), d_up.astype(BF16)
+        hiddens.append(hidden)
+        lefts, starts = (d_gate, d_up), (0, cols)
+        if last:
+            payload, scatter = product_to_mdl(lefts, weight, starts, partial)
+            rows, above, _ = lax.optimization_barrier((rows, above, payload[0]))
+        local = part_grad(rows, above, d_gate, d_up, hidden)
+        if not last:
+            d_gate = after(d_gate, local[0])
+            partial = (sum_products((d_gate, d_up), weight, starts),)
+            rows, above, _ = lax.optimization_barrier((rows, above, local[0]))
+        sums.append(pair_to_tok(local))
     d_two = scatter(payload)
     stat_two = sum_mdl(stat_two.reshape(8, -1)).reshape(-1, 1) * (1.0 / features)
     scale_mixed = scale_two * mixed
     cotangent_own = lax.dynamic_slice_in_dim(cotangent, me * width, width, 1).astype(F32)
     d_mixed = cotangent_own + scale_two * (d_two - scale_mixed * stat_two)
 
-    d_mixed_b = after(d_mixed.astype(BF16), up_local[0])
-    hidden_later = after(hidden, d_mixed_b)
-    ffn_payload, ffn_scatter = product_to_mdl((hidden_later,), w_down_t, (0,))
+    d_mixed_b = after(d_mixed.astype(BF16), local[0])
+    down_starts = tuple(2 * (stop - start) for start, stop in parts)
+    ffn = (sum_products((after(hiddens[0], d_mixed_b),), w_parts[0], down_starts[:1]),)
+    ffn_payload, ffn_scatter = product_to_mdl(
+        (after(hiddens[1], d_mixed_b),), w_parts[1], down_starts[1:], ffn
+    )
     if size == 4 and lax.axis_size("tok") == 8:
         pieces = gather_pieces(d_mixed_b)
         d_head = pieces_product(pieces, w_attn, qkv_cols, head_block.shape[1])
@@ -589,7 +666,6 @@
         out_local = pair_grad(d_mixed_rows, head_block)
     out_grad = pair_to_tok(out_local)
     d_attended = rows_to_cols(d_head)
-    block_out = (mixed + ffn_scatter(ffn_payload)).astype(BF16)
     d_query, d_kv = attention_backward(
         first, qkv, kv, cos, sin, pos, attended, d_attended, log_norm
     )
@@ -606,20 +682,27 @@
     *qkv_local, gain_one = pair_grad(rows_in, d_scaled, w_attn)
     qkv_sum = pair_to_tok(qkv_local)
     d_one = scatter(payload)
+    ffn_sum = ffn_scatter(ffn_payload)
+    block_out = (mixed + ffn_sum).astype(BF16)
     input_grad = d_mixed + scale_one * (d_one - (scale_one * residual) * stat_one)
 
     norm1_late, norm2_late, gate_late, up_late, _ = lax.optimization_barrier(
-        (norm1_gain, norm2_gain, gate_weight, up_weight, up_local[0])
+        (norm1_gain, norm2_gain, gate_weight, up_weight, local[0])
     )
 
     def unfold(total, gain):
         return total * gain.astype(F32)[:, None]
 
+    def joined(at):
+        widths = [total.shape[1] // 3 for total in sums]
+        pieces = [total[:, at * cols :][:, :cols] for total, cols in zip(sums, widths)]
+        return jnp.concatenate(pieces, axis=1)
+
+    gate_sum, up_sum, down_grad = joined(0), joined(1), joined(2).T
     gain_two = jnp.sum(
         gate_late.astype(F32) * gate_sum + up_late.astype(F32) * up_sum, axis=1
     )
     gate_grad, up_grad = unfold(gate_sum, norm2_late), unfold(up_sum, norm2_late)
-    down_grad = down_grad.T
     out_grad = out_grad.T
     gain_two_grad = sum_mdl(gain_two)
     gain_one = sum_mdl(sum_tok(gain_one.reshape(8, -1))).reshape(-1)

time: 910 us -> 903 us (level)
  waiting for transfers between devices: 442 us -> 407 us
  blocking collectives: 39 us -> 18.7 us
  local copies, waits for them, and re-layouts: 23.1 us -> 42.4 us
  Pallas kernels: 165 us -> 178 us
  starting transfers between devices: 58 us -> 68.5 us
    pallas_call x0 -> x4, Pallas kernels: none -> 77.8 us  [the longest x2 48.2 us: part_grad(): pl.pallas_call(part_kernel, grid=(pairs,), out_shape=(out, out), in_specs...]
    reduce_scatter x5 -> x4, waiting for transfers between devices: 39.5 us -> 87.6 us  [pair_to_tok(): lax.psum_scatter(both, 'tok', scatter_dimension=0, tiled=True, axis_index...]
    all_gather x3, waiting for transfers between devices: 69.1 us -> 21.7 us  [from_tok(): return lax.all_gather(weight, 'tok', axis=dim, tiled=True)]
    pallas_call x4 -> x1, Pallas kernels: 56.5 us -> 9.21 us  [pair_grad(): pl.pallas_call(pair_kernel, grid=(pairs,), out_shape=out_shape, in_specs=...]
    ppermute x44, waiting for transfers between devices: 277 us -> 240 us  [swap(): return lax.ppermute(block, 'mdl', [(i, i ^ distance) for i in range(size)])]
    all_to_all x2 -> x1, blocking collectives: 39 us -> 18.7 us  [cols_to_rows(): return lax.all_to_all(block, 'mdl', split_axis=1, concat_axis=0, tiled=True)]
    pallas_call x4, Pallas kernels: 68 us -> 49.8 us  [scatter_product(): pl.pallas_call(functools.partial(payload_kernel, starts), grid_spec=pltpu...]
    convert_element_type x5 -> x4, other arithmetic: 25.7 us -> 28.3 us  [pair_to_tok(): both = (kept.astype(F32) + got.astype(F32)).astype(BF16)]
  transfers between devices with their start and end apart: 62 -> 61, of which waited for: 34 -> 35; matrix products, arithmetic and copies ran while one was open for 15% -> 18% of each run, Pallas kernels for 15% -> 18%
where the time goes in v6:
time: 903 us; the launch traced here: 894 us
  waiting for transfers between devices  407 us (45%)
  Pallas kernels  178 us (20%)
  other arithmetic  95.3 us (11%)
  matrix products  68.8 us (8%)
  starting transfers between devices  68.5 us (8%)
  local copies, waits for them, and re-layouts  42.4 us (5%)
  blocking collectives  18.7 us (2%)
  between operations  15.6 us (2%)
    ppermute x44, waiting for transfers between devices, swap(): return lax.ppermute(block, 'mdl', [(i, i ^ distance) for i in range(size)])  240 us
    reduce_scatter x4, waiting for transfers between devices, pair_to_tok(): lax.psum_scatter(both, 'tok', scatter_dimension=0, tiled=True, axis_index...  87.6 us
    dot_general x7, matrix products, nn(): return jnp.dot(left_op, right_op, preferred_element_type=F32)  68.8 us
    ppermute x44, starting transfers between devices, swap(): return lax.ppermute(block, 'mdl', [(i, i ^ distance) for i in range(size)])  54.9 us
    pallas_call x4, Pallas kernels, scatter_product(): pl.pallas_call(functools.partial(payload_kernel, starts), grid_spec=pltpu...  49.8 us
    pallas_call x2, Pallas kernels, part_grad(): pl.pallas_call(part_kernel, grid=(pairs,), out_shape=(out, out), in_specs...  48.2 us
    all_to_all x2, waiting for transfers between devices, rows_to_cols(): return lax.all_to_all(block, 'mdl', split_axis=0, concat_axis=1, tiled=True)  36.8 us
    pallas_call x2, Pallas kernels, sum_products(): pl.pallas_call(functools.partial(sum_kernel, starts), grid=(rows // step,...  29.6 us
  transfers between devices with their start and end apart: 61, of which 35 were waited for; matrix products, arithmetic and copies ran while one was open for 18% of the time, Pallas kernels for 18%

profile of v6, /device:TPU:0, one launch (start us, length us, event | category | flops | bytes accessed | tf_op | source)
XLA Modules:
  0.0 894.0 jit_solution(1423287466931776233)
XLA Ops:
  17.5 3.0 collective-permute-start
  22.0 27.3 %collective-permute-done = bf16[1024,640]{1,0:T(8,128)(2,1)S(1)} collective-permute-done((bf16[1024,640]{1,0:T(8,128)(2,1)S(1)}, bf16[1024,640]{1,0:T(8,128)(2,1)S(1)}, u32[]{:S(2)}, u32[]{:S(2)}) %collective-permute-start) | collective-permute-done | bytes 1310752 | tf_op jit(solution)/shard_map/ppermute | solution.py:38
  57.3 9.1 %collective-permute-done.2 = bf16[512,640]{1,0:T(8,128)(2,1)S(1)} collective-permute-done((bf16[512,640]{1,0:T(8,128)(2,1)}, bf16[512,640]{1,0:T(8,128)(2,1)S(1)}, u32[]{:S(2)}, u32[]{:S(2)}) %collective-permute-start.2) | collective-permute-done | bytes 655392 | tf_op jit(solution)/shard_map/ppermute | solution.py:38
  66.5 3.2 collective-permute-done.3
  73.2 13.2 %all-gather.4.cloned.1.call-done.refs_1_.weight_ref.refs_0_ = bf16[2560,1408]{1,0:T(8,128)(2,1)} async-done(((bf16[320,1408]{1,0:T(8,128)(2,1)}), bf16[2560,1408]{1,0:T(8,128)(2,1)}) %all-gather.4.cloned.1.call-update) | async-done | bytes 7208976 | tf_op jit(solution)/shard_map/all_gather | solution.py:575
  86.4 9.0 %multiply_convert_fusion.3 = bf16[1024,768]{1,0:T(8,128)(2,1)} fusion(bf16[1024,2560]{1,0:T(8,128)(2,1)} %copy-done.34, bf16[2560,1408]{1,0:T(8,128)(2,1)} %all-gather.4.cloned.1.call-done.refs_1_.weight_ref.refs_0_, f32[1024]{0:T(1024)S(1)} %add_rsqrt_fusion.1), kind=kOutput, calls=%fused_computation.43 | convolution fusion | flops 4028104704 | bytes 10752000 | tf_op jit(solution)/shard_map/dot_general | solution.py:33
  95.5 3.8 all-to-all-start
  99.4 19.7 %all-to-all-done = bf16[4,256,768]{2,1,0:T(8,128)(2,1)S(1)} async-done(((bf16[4,256,768]{2,1,0:T(8,128)(2,1)}), bf16[4,256,768]{2,1,0:T(8,128)(2,1)S(1)}, u32[]{:S(2)}, u32[]{:S(2)}) %all-to-all-start) | async-done | bytes 1572896 | tf_op jit(solution)/shard_map/all_to_all | solution.py:142
  123.8 5.6 collective-permute-done.4
  131.7 2.8 collective-permute-done.6
  136.1 10.8 %attention_forward.1 = (bf16[256,2560]{1,0:T(8,128)(2,1)S(1)}, f32[10,256,1]{2,1,0:T(8,128)S(1)}) custom-call(s32[1]{0:T(128)} %bitcast.1.first_ref, bf16[256,3072]{1,0:T(8,128)(2,1)S(1)} %bitcast.131, bf16[1024,512]{1,0:T(8,128)(2,1)S(1)} %constant_dynamic-update-slice_fusion.4.kv_ref, f32[256,128]{1,0:T(8,128)S(1)} %get-tuple-element.137.cos_ref, ...), custom_call_target="tpu_custom_call" | custom-call | flops 2684354560 | bytes 3670016 | tf_op jit(solution)/shard_map/attention_forward/pallas_call | solution.py:225
  147.1 18.7 %all_to_all.76 = bf16[256,4,640]{2,0,1:T(8,128)(2,1)} all-to-all(bf16[256,4,640]{2,0,1:T(8,128)(2,1)S(1)} %bitcast.141), channel_id=1, replica_groups=mesh['tok'=8,'mdl'=4] {'mdl'}, dimensions={1} | all-to-all | bytes 2621440 | tf_op jit(solution)/shard_map/all_to_all | solution.py:146
  165.8 7.9 shard_map.169
  175.2 25.6 %collective-permute-done.8 = bf16[2,512,640]{2,1,0:T(8,128)(2,1)S(1)} collective-permute-done((bf16[2,512,640]{2,1,0:T(8,128)(2,1)S(1)}, bf16[2,512,640]{2,1,0:T(8,128)(2,1)S(1)}, u32[]{:S(2)}, u32[]{:S(2)}) %collective-permute-start.8) | collective-permute-done | bytes 1310752 | tf_op jit(solution)/shard_map/ppermute | solution.py:38
  204.7 11.2 %collective-permute-done.9 = bf16[512,640]{1,0:T(8,128)(2,1)S(1)} collective-permute-done((bf16[512,640]{1,0:T(8,128)(2,1)S(1)}, bf16[512,640]{1,0:T(8,128)(2,1)S(1)}, u32[]{:S(2)}, u32[]{:S(2)}) %collective-permute-start.9) | collective-permute-done | bytes 655392 | tf_op jit(solution)/shard_map/ppermute | solution.py:38
  222.8 26.1 %collective-permute-done.12 = bf16[1024,640]{1,0:T(8,128)(2,1)S(1)} collective-permute-done((bf16[1024,640]{1,0:T(8,128)(2,1)S(1)}, bf16[1024,640]{1,0:T(8,128)(2,1)S(1)}, u32[]{:S(2)}, u32[]{:S(2)}) %collective-permute-start.12) | collective-permute-done | bytes 1310752 | tf_op jit(solution)/shard_map/ppermute | solution.py:38
  258.7 5.4 collective-permute-done.14
  268.4 3.6 fusion
  272.0 5.8 fusion.1.rows_ref
  277.9 9.1 %fusion.2 = f32[1024,1024]{1,0:T(8,128)S(1)} fusion(bf16[1024,2560]{1,0:T(8,128)(2,1)} %fusion.1.rows_ref, bf16[2560,3072]{1,0:T(8,128)(2,1)} %all-gather.6.cloned.1.call-done.refs_2_.refs_1_), kind=kOutput, calls=%fused_computation.7 | convolution fusion | flops 5368709120 | bytes 14680064 | tf_op jit(solution)/shard_map/dot_general | solution.py:33
  286.9 9.2 %fusion.6 = f32[1024,1024]{0,1:T(8,128)S(1)} fusion(bf16[1024,2560]{1,0:T(8,128)(2,1)} %above_ref.2, bf16[2560,3072]{1,0:T(8,128)(2,1)} %all-gather.6.cloned.1.call-done.refs_2_.refs_1_), kind=kOutput, calls=%fused_computation.11 | convolution fusion | flops 5368709120 | bytes 14680064 | tf_op jit(solution)/shard_map/dot_general | solution.py:33
  296.2 11.6 %add_reduce_fusion = (f32[1024]{0:T(1024)S(1)}, bf16[1024,1024]{1,0:T(8,128)(2,1)S(1)}, bf16[1024,1024]{1,0:T(8,128)(2,1)S(1)}, bf16[1024,1024]{1,0:T(8,128)(2,1)}) fusion(f32[1024,1024]{1,0:T(8,128)S(1)} %fusion.2, f32[1024,1024]{0,1:T(8,128)S(1)} %fusion.6, bf16[1024,2560]{1,0:T(8,128)(2,1)S(1)} %copy-done.40, ...), kind=kOutput, calls=%fused_computation.22 | convolution fusion | flops 5398068224 | bytes 25169920 | tf_op jit(solution)/shard_map/dot_general | solution.py:33
  307.8 24.6 %shard_map.170 = (bf16[1280,3072]{1,0:T(8,128)(2,1)}, bf16[1280,3072]{1,0:T(8,128)(2,1)}) custom-call(s32[1]{0:T(128)} %bitcast.12.core_ref, bf16[1024,2560]{1,0:T(8,128)(2,1)} %fusion.1.rows_ref, bf16[1024,2560]{1,0:T(8,128)(2,1)} %above_ref.2, bf16[1024,1024]{1,0:T(8,128)(2,1)S(1)} %get-tuple-element.60.d_gate_ref.refs_0_, ...), custom_call_target="tpu_custom_call" | custom-call | flops 16106127360 | bytes 32505856 | tf_op jit(solution)/shard_map/pallas_call | solution.py:363
  332.4 15.7 %shard_map.171.refs_3_ = f32[1024,2560]{1,0:T(8,128)} custom-call(bf16[1024,1024]{1,0:T(8,128)(2,1)S(1)} %get-tuple-element.60.d_gate_ref.refs_0_, bf16[1024,1024]{1,0:T(8,128)(2,1)S(1)} %get-tuple-element.103.d_up_ref.refs_1_, bf16[2560,3072]{1,0:T(8,128)(2,1)} %all-gather.6.cloned.1.call-done.refs_2_.refs_1_), custom_call_target="tpu_custom_call" | custom-call | flops 10737418240 | bytes 26214400 | tf_op jit(solution)/shard_map/pallas_call | solution.py:435
  348.1 8.5 all-gather.8.cloned.1.call-done.refs_2_.refs_1_
  356.6 9.0 %fusion.10 = f32[1024,896]{1,0:T(8,128)S(1)} fusion(bf16[1024,2560]{1,0:T(8,128)(2,1)} %fusion.1.rows_ref, bf16[2560,2688]{1,0:T(8,128)(2,1)} %all-gather.8.cloned.1.call-done.refs_2_.refs_1_), kind=kOutput, calls=%fused_computation.15 | convolution fusion | flops 4697620480 | bytes 13500416 | tf_op jit(solution)/shard_map/dot_general | solution.py:33
  365.6 8.9 fusion.8
  374.5 12.0 %fusion.67 = (bf16[1024,896]{1,0:T(8,128)(2,1)}, f32[1024]{0:T(1024)S(1)}, bf16[1024,896]{1,0:T(8,128)(2,1)}, bf16[1024,896]{1,0:T(8,128)(2,1)S(1)}) fusion(f32[1024,896]{1,0:T(8,128)S(1)} %fusion.8, f32[1024,896]{1,0:T(8,128)S(1)} %fusion.10, bf16[1024,2560]{1,0:T(8,128)(2,1)S(1)} %bitcast.140, ...), kind=kOutput, calls=%fused_computation.173 | convolution fusion | flops 4723309568 | bytes 22679552 | tf_op jit(solution)/shard_map/dot_general | solution.py:33
  386.5 18.4 %shard_map.172 = (bf16[2,512,640]{2,1,0:T(8,128)(2,1)S(1)}, bf16[2,512,640]{2,1,0:T(8,128)(2,1)S(1)}, bf16[2,512,640]{2,1,0:T(8,128)(2,1)S(1)}, bf16[2,512,640]{2,1,0:T(8,128)(2,1)S(1)}) custom-call(s32[1]{0:T(128)} %bitcast.me_ref, bf16[1024,896]{1,0:T(8,128)(2,1)} %get-tuple-element.101.refs_0_.d_gate_ref, ...), custom_call_target="tpu_custom_call" | custom-call | flops 9395240960 | bytes 22675456 | tf_op jit(solution)/shard_map/pallas_call | solution.py:476
  408.6 27.5 %collective-permute-done.20 = f32[8,128]{1,0:T(8,128)S(1)} collective-permute-done((f32[8,128]{1,0:T(8,128)S(1)}, f32[8,128]{1,0:T(8,128)S(1)}, u32[]{:S(2)}, u32[]{:S(2)}) %collective-permute-start.20) | collective-permute-done | bytes 4128 | tf_op jit(solution)/shard_map/ppermute | solution.py:38
  441.1 23.6 %shard_map.173 = (bf16[1280,2688]{1,0:T(8,128)(2,1)}, bf16[1280,2688]{1,0:T(8,128)(2,1)}) custom-call(s32[1]{0:T(128)} %bitcast.12.core_ref, bf16[1024,2560]{1,0:T(8,128)(2,1)} %fusion.1.rows_ref, bf16[1024,2560]{1,0:T(8,128)(2,1)} %above_ref.2, bf16[1024,896]{1,0:T(8,128)(2,1)S(1)} %copy-done.21, bf16[1024,896]{1,0:T(8,128)(2,1)S(1)} %copy-done.22, ...), custom_call_target="tpu_custom_call" | custom-call | flops 14092861440 | bytes 29753344 | tf_op jit(solution)/shard_map/pallas_call | solution.py:363
  466.6 4.0 fusion.68
  472.4 29.4 %collective-permute-done.26.along_x = bf16[1024,640]{1,0:T(8,128)(2,1)S(1)} collective-permute-done((bf16[1024,640]{1,0:T(8,128)(2,1)S(1)}, bf16[1024,640]{1,0:T(8,128)(2,1)S(1)}, u32[]{:S(2)}, u32[]{:S(2)}) %collective-permute-start.26) | collective-permute-done | bytes 1310752 | tf_op jit(solution)/shard_map/ppermute | solution.py:38
  503.8 14.4 %collective-permute-done.28.top = bf16[512,640]{1,0:T(8,128)(2,1)S(1)} collective-permute-done((bf16[512,640]{1,0:T(8,128)(2,1)S(1)}, bf16[512,640]{1,0:T(8,128)(2,1)S(1)}, u32[]{:S(2)}, u32[]{:S(2)}) %collective-permute-start.28) | collective-permute-done | bytes 655392 | tf_op jit(solution)/shard_map/ppermute | solution.py:38
  519.3 6.8 shard_map.176
  526.1 7.6 shard_map.179
  533.7 3.7 collective-permute-done.46
  537.4 3.0 add_convert_fusion.3
  540.5 9.7 %add_convert_fusion.1 = bf16[1280,2688]{1,0:T(8,128)(2,1)} fusion(bf16[1280,2688]{1,0:T(8,128)(2,1)} %collective-permute-done.48, bf16[1280,2688]{1,0:T(8,128)(2,1)} %get-tuple-element.67), kind=kLoop, calls=%fused_computation.1 | loop fusion | flops 13762560 | bytes 20643840 | tf_op jit(solution)/shard_map/convert_element_type | solution.py:581
  550.7 12.6 %collective-permute-done.47 = bf16[1280,3072]{1,0:T(8,128)(2,1)} collective-permute-done((bf16[1280,3072]{1,0:T(8,128)(2,1)}, bf16[1280,3072]{1,0:T(8,128)(2,1)}, u32[]{:S(2)}, u32[]{:S(2)}) %collective-permute-start.47) | collective-permute-done | bytes 7864352 | tf_op jit(solution)/shard_map/ppermute | solution.py:580
  563.3 12.2 %add_convert_fusion = bf16[1280,3072]{1,0:T(8,128)(2,1)} fusion(bf16[1280,3072]{1,0:T(8,128)(2,1)} %collective-permute-done.47, bf16[1280,3072]{1,0:T(8,128)(2,1)} %get-tuple-element.57), kind=kLoop, calls=%fused_computation | loop fusion | flops 15728640 | bytes 23592960 | tf_op jit(solution)/shard_map/convert_element_type | solution.py:581
  575.6 4.5 all-to-all-start.2
  580.1 17.1 %all-to-all-done.2 = bf16[4,256,640]{2,1,0:T(8,128)(2,1)} async-done(((bf16[4,256,640]{2,1,0:T(8,128)(2,1)}), bf16[4,256,640]{2,1,0:T(8,128)(2,1)}, u32[]{:S(2)}, u32[]{:S(2)}) %all-to-all-start.2) | async-done | bytes 1310752 | tf_op jit(solution)/shard_map/all_to_all | solution.py:142
  599.2 15.7 %attention_backward.1 = (bf16[256,2560]{1,0:T(8,128)(2,1)S(1)}, f32[1024,512]{1,0:T(8,128)S(1)}) custom-call(s32[1]{0:T(128)} %bitcast.1.first_ref, bf16[256,3072]{1,0:T(8,128)(2,1)S(1)} %bitcast.132, bf16[1024,512]{1,0:T(8,128)(2,1)S(1)} %copy-done.14, f32[256,128]{1,0:T(8,128)S(1)} %copy-done.20, f32[256,128]{1,0:T(8,128)S(1)} %copy-done.18, ...), custom_call_target="tpu_custom_call" | custom-call | flops 6710886400 | bytes 8388608 | tf_op jit(solution)/shard_map/attention_backward/pallas_call | solution.py:250
  617.4 5.3 collective-permute-done.30
  624.3 3.5 collective-permute-done.31
  629.4 3.5 collective-permute-done.33
  636.2 4.4 all-to-all-start.3
  640.9 14.0 %shard_map.174.refs_2_ = f32[1024,2560]{1,0:T(8,128)} custom-call(bf16[1024,1024]{1,0:T(8,128)(2,1)S(1)} %copy-done, bf16[2560,3072]{1,0:T(8,128)(2,1)} %all-gather.6.cloned.1.call-done.refs_2_.refs_1_), custom_call_target="tpu_custom_call" | custom-call | flops 5368709120 | bytes 26214400 | tf_op jit(solution)/shard_map/pallas_call | solution.py:435
  654.8 13.7 %shard_map.175 = (bf16[2,512,640]{2,1,0:T(8,128)(2,1)}, bf16[2,512,640]{2,1,0:T(8,128)(2,1)}, bf16[2,512,640]{2,1,0:T(8,128)(2,1)S(1)}, bf16[2,512,640]{2,1,0:T(8,128)(2,1)S(1)}) custom-call(s32[1]{0:T(128)} %bitcast.me_ref, bf16[1024,896]{1,0:T(8,128)(2,1)} %copy-done.1, bf16[2560,2688]{1,0:T(8,128)(2,1)} %all-gather.8.cloned.1.call-done.refs_2_.refs_1_, ...), custom_call_target="tpu_custom_call" | custom-call | flops 4697620480 | bytes 20840448 | tf_op jit(solution)/shard_map/pallas_call | solution.py:476
  674.0 9.8 %shard_map.177 = (bf16[2,512,640]{2,1,0:T(8,128)(2,1)}, bf16[2,512,640]{2,1,0:T(8,128)(2,1)}, bf16[2,512,640]{2,1,0:T(8,128)(2,1)S(1)}, bf16[2,512,640]{2,1,0:T(8,128)(2,1)S(1)}) custom-call(s32[1]{0:T(128)} %bitcast.me_ref, bf16[1024,768]{1,0:T(8,128)(2,1)} %bitcast.37.refs_0_, bf16[2560,1408]{1,0:T(8,128)(2,1)} %all-gather.4.cloned.1.call-done.refs_1_.weight_ref.refs_0_), custom_call_target="tpu_custom_call" | custom-call | flops 4026531840 | bytes 14024704 | tf_op jit(solution)/shard_map/pallas_call | solution.py:476
  687.2 9.2 %shard_map.178 = (bf16[1280,768]{1,0:T(8,128)(2,1)S(1)}, bf16[1280,768]{1,0:T(8,128)(2,1)}, f32[2560,1]{1,0:T(8,128)S(1)}) custom-call(s32[1]{0:T(128)} %bitcast.12.core_ref, bf16[1024,2560]{1,0:T(8,128)(2,1)} %copy-done.34, bf16[1024,768]{1,0:T(8,128)(2,1)S(1)} %multiply_convert_fusion.2.right_ref, ...), custom_call_target="tpu_custom_call" | custom-call | flops 4026531840 | bytes 10747904 | tf_op jit(solution)/shard_map/pallas_call | solution.py:330
  708.6 7.3 collective-permute-done.23
  716.0 2.8 bitcast_add_fusion.3
  726.7 3.3 add_convert_fusion.2
  730.1 2.9 bitcast_add_fusion.2
  736.6 11.3 %collective-permute-done.38 = f32[4,256]{1,0:T(4,128)S(1)} collective-permute-done((f32[4,256]{1,0:T(4,128)S(1)}, f32[4,256]{1,0:T(4,128)S(1)}, u32[]{:S(2)}, u32[]{:S(2)}) %collective-permute-start.38) | collective-permute-done | bytes 4128 | tf_op jit(solution)/shard_map/ppermute | solution.py:38
  760.9 9.2 %collective-permute-done.35 = bf16[512,640]{1,0:T(8,128)(2,1)S(1)} collective-permute-done((bf16[512,640]{1,0:T(8,128)(2,1)}, bf16[512,640]{1,0:T(8,128)(2,1)S(1)}, u32[]{:S(2)}, u32[]{:S(2)}) %collective-permute-start.35) | collective-permute-done | bytes 655392 | tf_op jit(solution)/shard_map/ppermute | solution.py:38
  775.6 4.5 fusion.22
  782.0 3.2 fusion.72
  785.3 49.6 %reduce-scatter.9.cloned.1.call-done = bf16[320,3072]{1,0:T(8,128)(2,1)} async-done(((bf16[1280,3072]{1,0:T(8,128)(2,1)}), bf16[320,3072]{1,0:T(8,128)(2,1)}) %reduce-scatter.9.cloned.1.call-update) | async-done | bytes 1966096 | tf_op jit(solution)/shard_map/reduce_scatter | solution.py:583
  837.4 2.9 fusion.26
  841.9 38.0 %reduce-scatter.5.cloned.1.call-done = bf16[320,768]{1,0:T(8,128)(2,1)} async-done(((bf16[1280,768]{1,0:T(8,128)(2,1)}), bf16[320,768]{1,0:T(8,128)(2,1)}) %reduce-scatter.5.cloned.1.call-update) | async-done | bytes 491536 | tf_op jit(solution)/shard_map/reduce_scatter | solution.py:583
  883.4 2.9 maximum_bitcast_fusion
  (346 shorter events, 146.6 us)
Async XLA Ops:
  7.2 79.2 %all-gather.4.cloned.1.call-start = ((), (), s32[]{:S(2)}) async-start(), calls=%async_computation.8 | async-start | bytes 8110080 | tf_op jit(solution)/shard_map/all_gather | solution.py:575
  11.3 266.6 %all-gather.6.cloned.1.call-start = ((), (), s32[]{:S(2)}) async-start(), calls=%async_computation.9 | async-start | bytes 17694720 | tf_op jit(solution)/shard_map/all_gather | solution.py:575
  14.2 342.4 %all-gather.8.cloned.1.call-start = ((), (), s32[]{:S(2)}) async-start(), calls=%async_computation.10 | async-start | bytes 15482880 | tf_op jit(solution)/shard_map/all_gather | solution.py:575
  17.5 31.7 %collective-permute-start = (bf16[1024,640]{1,0:T(8,128)(2,1)S(1)}, bf16[1024,640]{1,0:T(8,128)(2,1)S(1)}, u32[]{:S(2)}, u32[]{:S(2)}) collective-permute-start(bf16[1024,640]{1,0:T(8,128)(2,1)S(1)} %copy-done.30), channel_id=1, source_target_pairs={{0,1},{1,0},{2,3},{3,2},{4,5},{5,4},{6,7},{7,6},{8,9},{9,8},{10,11... | collective-permute-start | bytes 3932168 | tf_op jit(solution)/shard_map/ppermute | solution.py:38
  20.5 31.4 %collective-permute-start.1 = (bf16[1024,640]{1,0:T(8,128)(2,1)S(1)}, bf16[1024,640]{1,0:T(8,128)(2,1)S(1)}, u32[]{:S(2)}, u32[]{:S(2)}) collective-permute-start(bf16[1024,640]{1,0:T(8,128)(2,1)S(1)} %copy-done.30), channel_id=1, source_target_pairs={{0,2},{1,3},{2,0},{3,1},{4,6},{5,7},{6,4},{7,5},{8,10},{9,11},{10,... | collective-permute-start | bytes 3932168 | tf_op jit(solution)/shard_map/ppermute | solution.py:38
  50.2 16.2 %collective-permute-start.2 = (bf16[512,640]{1,0:T(8,128)(2,1)}, bf16[512,640]{1,0:T(8,128)(2,1)S(1)}, u32[]{:S(2)}, u32[]{:S(2)}) collective-permute-start(bf16[512,640]{1,0:T(8,128)(2,1)} %slice.288), channel_id=1, source_target_pairs={{0,2},{1,3},{2,0},{3,1},{4,6},{5,7},{6,4},{7,5},{8,10},{9,11},{10,... | collective-permute-start | bytes 1966088 | tf_op jit(solution)/shard_map/ppermute | solution.py:38
  53.9 15.8 %collective-permute-start.3 = (bf16[512,640]{1,0:T(8,128)(2,1)}, bf16[512,640]{1,0:T(8,128)(2,1)}, u32[]{:S(2)}, u32[]{:S(2)}) collective-permute-start(bf16[512,640]{1,0:T(8,128)(2,1)} %slice.289), channel_id=1, source_target_pairs={{0,1},{1,0},{2,3},{3,2},{4,5},{5,4},{6,7},{7,6},{8,9},{9,8},{10,11... | collective-permute-start | bytes 1966088 | tf_op jit(solution)/shard_map/ppermute | solution.py:38
  95.5 23.6 %all-to-all-start = ((bf16[4,256,768]{2,1,0:T(8,128)(2,1)}), bf16[4,256,768]{2,1,0:T(8,128)(2,1)S(1)}, u32[]{:S(2)}, u32[]{:S(2)}) async-start(bf16[4,256,768]{2,1,0:T(8,128)(2,1)} %bitcast.3), calls=%async_computation | async-start | bytes 3145728 | tf_op jit(solution)/shard_map/all_to_all | solution.py:142
  99.3 680.8 %reduce-scatter.7.cloned.1.call-start = ((), (), s32[]{:S(2)}) async-start(), calls=%async_computation.12 | async-start | bytes 2048000 | tf_op jit(solution)/shard_map/reduce_scatter | solution.py:583
  121.7 7.8 collective-permute-start.4
  123.1 7.9 collective-permute-start.5
  129.5 5.0 collective-permute-start.6
  131.0 5.0 collective-permute-start.7
  173.7 27.1 %collective-permute-start.8 = (bf16[2,512,640]{2,1,0:T(8,128)(2,1)S(1)}, bf16[2,512,640]{2,1,0:T(8,128)(2,1)S(1)}, u32[]{:S(2)}, u32[]{:S(2)}) collective-permute-start(bf16[2,512,640]{2,1,0:T(8,128)(2,1)S(1)} %get-tuple-element.54), channel_id=1, source_target_pairs={{0,1},{1,0},{2,3},{3,2},{4,5},{5,4},{6,7},{7,6},{8,9},{9,8},{10,11... | collective-permute-start | bytes 3932168 | tf_op jit(solution)/shard_map/ppermute | solution.py:38
  174.8 29.6 %collective-permute-start.10 = (bf16[2,512,640]{2,1,0:T(8,128)(2,1)S(1)}, bf16[2,512,640]{2,1,0:T(8,128)(2,1)S(1)}, u32[]{:S(2)}, u32[]{:S(2)}) collective-permute-start(bf16[2,512,640]{2,1,0:T(8,128)(2,1)S(1)} %get-tuple-element.56), channel_id=1, source_target_pairs={{0,2},{1,3},{2,0},{3,1},{4,6},{5,7},{6,4},{7,5},{8,10},{9,11},{10,... | collective-permute-start | bytes 3932168 | tf_op jit(solution)/shard_map/ppermute | solution.py:38
  201.0 14.9 %collective-permute-start.9 = (bf16[512,640]{1,0:T(8,128)(2,1)S(1)}, bf16[512,640]{1,0:T(8,128)(2,1)S(1)}, u32[]{:S(2)}, u32[]{:S(2)}) collective-permute-start(bf16[512,640]{1,0:T(8,128)(2,1)S(1)} %fusion.33), channel_id=1, source_target_pairs={{0,2},{1,3},{2,0},{3,1},{4,6},{5,7},{6,4},{7,5},{8,10},{9,11},{10,... | collective-permute-start | bytes 1966088 | tf_op jit(solution)/shard_map/ppermute | solution.py:38
  204.6 11.5 %collective-permute-start.11 = (bf16[512,640]{1,0:T(8,128)(2,1)S(1)}, bf16[512,640]{1,0:T(8,128)(2,1)S(1)}, u32[]{:S(2)}, u32[]{:S(2)}) collective-permute-start(bf16[512,640]{1,0:T(8,128)(2,1)S(1)} %fusion.34), channel_id=1, source_target_pairs={{0,1},{1,0},{2,3},{3,2},{4,5},{5,4},{6,7},{7,6},{8,9},{9,8},{10,11... | collective-permute-start | bytes 1966088 | tf_op jit(solution)/shard_map/ppermute | solution.py:38
  216.1 249.2 %copy-start.25 = (f32[512,640]{1,0:T(8,128)}, f32[512,640]{1,0:T(8,128)S(1)}, u32[]{:S(2)}) copy-start(f32[512,640]{1,0:T(8,128)S(1)} %bitcast_add_fusion.7) | copy-start | bytes 3932164
  220.9 28.0 %collective-permute-start.12 = (bf16[1024,640]{1,0:T(8,128)(2,1)S(1)}, bf16[1024,640]{1,0:T(8,128)(2,1)S(1)}, u32[]{:S(2)}, u32[]{:S(2)}) collective-permute-start(bf16[1024,640]{1,0:T(8,128)(2,1)S(1)} %get-tuple-element.98), channel_id=1, source_target_pairs={{0,1},{1,0},{2,3},{3,2},{4,5},{5,4},{6,7},{7,6},{8,9},{9,8},{10,11... | collective-permute-start | bytes 3932168 | tf_op jit(solution)/shard_map/ppermute | solution.py:38
  221.5 29.6 %collective-permute-start.13 = (bf16[1024,640]{1,0:T(8,128)(2,1)S(1)}, bf16[1024,640]{1,0:T(8,128)(2,1)S(1)}, u32[]{:S(2)}, u32[]{:S(2)}) collective-permute-start(bf16[1024,640]{1,0:T(8,128)(2,1)S(1)} %get-tuple-element.98), channel_id=1, source_target_pairs={{0,2},{1,3},{2,0},{3,1},{4,6},{5,7},{6,4},{7,5},{8,10},{9,11},{10,... | collective-permute-start | bytes 3932168 | tf_op jit(solution)/shard_map/ppermute | solution.py:38
  250.8 13.4 %collective-permute-start.14 = (bf16[512,640]{1,0:T(8,128)(2,1)}, bf16[512,640]{1,0:T(8,128)(2,1)S(1)}, u32[]{:S(2)}, u32[]{:S(2)}) collective-permute-start(bf16[512,640]{1,0:T(8,128)(2,1)} %slice.301), channel_id=1, source_target_pairs={{0,2},{1,3},{2,0},{3,1},{4,6},{5,7},{6,4},{7,5},{8,10},{9,11},{10,... | collective-permute-start | bytes 1966088 | tf_op jit(solution)/shard_map/ppermute | solution.py:38
  253.1 13.4 %collective-permute-start.15 = (bf16[512,640]{1,0:T(8,128)(2,1)}, bf16[512,640]{1,0:T(8,128)(2,1)}, u32[]{:S(2)}, u32[]{:S(2)}) collective-permute-start(bf16[512,640]{1,0:T(8,128)(2,1)} %slice.302), channel_id=1, source_target_pairs={{0,1},{1,0},{2,3},{3,2},{4,5},{5,4},{6,7},{7,6},{8,9},{9,8},{10,11... | collective-permute-start | bytes 1966088 | tf_op jit(solution)/shard_map/ppermute | solution.py:38
  386.5 54.6 %copy-start.1 = (bf16[1024,896]{1,0:T(8,128)(2,1)}, bf16[1024,896]{1,0:T(8,128)(2,1)S(1)}, u32[]{:S(2)}) copy-start(bf16[1024,896]{1,0:T(8,128)(2,1)S(1)} %get-tuple-element.69.hidden_ref.refs_0_) | copy-start | bytes 5505028
  405.0 32.6 %collective-permute-start.16 = (bf16[2,512,640]{2,1,0:T(8,128)(2,1)S(1)}, bf16[2,512,640]{2,1,0:T(8,128)(2,1)S(1)}, u32[]{:S(2)}, u32[]{:S(2)}) collective-permute-start(bf16[2,512,640]{2,1,0:T(8,128)(2,1)S(1)} %get-tuple-element.62), channel_id=1, source_target_pairs={{0,1},{1,0},{2,3},{3,2},{4,5},{5,4},{6,7},{7,6},{8,9},{9,8},{10,11... | collective-permute-start | bytes 3932168 | tf_op jit(solution)/shard_map/ppermute | solution.py:38
  406.5 31.8 %collective-permute-start.18 = (bf16[2,512,640]{2,1,0:T(8,128)(2,1)S(1)}, bf16[2,512,640]{2,1,0:T(8,128)(2,1)S(1)}, u32[]{:S(2)}, u32[]{:S(2)}) collective-permute-start(bf16[2,512,640]{2,1,0:T(8,128)(2,1)S(1)} %get-tuple-element.64), channel_id=1, source_target_pairs={{0,2},{1,3},{2,0},{3,1},{4,6},{5,7},{6,4},{7,5},{8,10},{9,11},{10,... | collective-permute-start | bytes 3932168 | tf_op jit(solution)/shard_map/ppermute | solution.py:38
  408.0 28.1 %collective-permute-start.20 = (f32[8,128]{1,0:T(8,128)S(1)}, f32[8,128]{1,0:T(8,128)S(1)}, u32[]{:S(2)}, u32[]{:S(2)}) collective-permute-start(f32[8,128]{1,0:T(8,128)S(1)} %add_bitcast_fusion), channel_id=1, source_target_pairs={{0,1},{1,0},{2,3},{3,2},{4,5},{5,4},{6,7},{7,6},{8,9},{9,8},{10,11... | collective-permute-start | bytes 12296 | tf_op jit(solution)/shard_map/ppermute | solution.py:38
  436.1 28.6 %collective-permute-start.21 = (f32[8,128]{1,0:T(8,128)S(1)}, f32[8,128]{1,0:T(8,128)S(1)}, u32[]{:S(2)}, u32[]{:S(2)}) collective-permute-start(f32[8,128]{1,0:T(8,128)S(1)} %fusion.80), channel_id=1, source_target_pairs={{0,2},{1,3},{2,0},{3,1},{4,6},{5,7},{6,4},{7,5},{8,10},{9,11},{10,... | collective-permute-start | bytes 12296 | tf_op jit(solution)/shard_map/ppermute | solution.py:38
  437.7 27.0 %collective-permute-start.17 = (bf16[512,640]{1,0:T(8,128)(2,1)S(1)}, bf16[512,640]{1,0:T(8,128)(2,1)S(1)}, u32[]{:S(2)}, u32[]{:S(2)}) collective-permute-start(bf16[512,640]{1,0:T(8,128)(2,1)S(1)} %fusion.35), channel_id=1, source_target_pairs={{0,2},{1,3},{2,0},{3,1},{4,6},{5,7},{6,4},{7,5},{8,10},{9,11},{10,... | collective-permute-start | bytes 1966088 | tf_op jit(solution)/shard_map/ppermute | solution.py:38
  439.6 25.3 %collective-permute-start.19 = (bf16[512,640]{1,0:T(8,128)(2,1)}, bf16[512,640]{1,0:T(8,128)(2,1)S(1)}, u32[]{:S(2)}, u32[]{:S(2)}) collective-permute-start(bf16[512,640]{1,0:T(8,128)(2,1)} %fusion.36), channel_id=1, source_target_pairs={{0,1},{1,0},{2,3},{3,2},{4,5},{5,4},{6,7},{7,6},{8,9},{9,8},{10,11... | collective-permute-start | bytes 1966088 | tf_op jit(solution)/shard_map/ppermute | solution.py:38
  464.7 75.9 %collective-permute-start.48 = (bf16[1280,2688]{1,0:T(8,128)(2,1)}, bf16[1280,2688]{1,0:T(8,128)(2,1)}, u32[]{:S(2)}, u32[]{:S(2)}) collective-permute-start(bf16[1280,2688]{1,0:T(8,128)(2,1)} %get-tuple-element.92), channel_id=1, source_target_pairs={{0,4},{4,0},{8,12},{12,8},{16,20},{20,16},{24,28},{28,24},{1,5},{5... | collective-permute-start | bytes 20643848 | tf_op jit(solution)/shard_map/ppermute | solution.py:580
  465.0 54.3 %slice-start = ((s8[7208960]{0:T(1024)(128)(4,1)}), s8[4194304]{0:T(1024)(128)(4,1)S(1)}, s32[]{:S(2)}) async-start(s8[7208960]{0:T(1024)(128)(4,1)} %bitcast.128), calls=%async_computation.15 | async-start | bytes 8388608
  470.6 31.2 %collective-permute-start.26 = (bf16[1024,640]{1,0:T(8,128)(2,1)S(1)}, bf16[1024,640]{1,0:T(8,128)(2,1)S(1)}, u32[]{:S(2)}, u32[]{:S(2)}) collective-permute-start(bf16[1024,640]{1,0:T(8,128)(2,1)S(1)} %get-tuple-element.68.own), channel_id=1, source_target_pairs={{0,1},{1,0},{2,3},{3,2},{4,5},{5,4},{6,7},{7,6},{8,9},{9,8},{10,11... | collective-permute-start | bytes 3932168 | tf_op jit(solution)/shard_map/ppermute | solution.py:38
  471.2 31.9 %collective-permute-start.27 = (bf16[1024,640]{1,0:T(8,128)(2,1)S(1)}, bf16[1024,640]{1,0:T(8,128)(2,1)S(1)}, u32[]{:S(2)}, u32[]{:S(2)}) collective-permute-start(bf16[1024,640]{1,0:T(8,128)(2,1)S(1)} %get-tuple-element.68.own), channel_id=1, source_target_pairs={{0,2},{1,3},{2,0},{3,1},{4,6},{5,7},{6,4},{7,5},{8,10},{9,11},{10,... | collective-permute-start | bytes 3932168 | tf_op jit(solution)/shard_map/ppermute | solution.py:38
  501.9 16.3 %collective-permute-start.28 = (bf16[512,640]{1,0:T(8,128)(2,1)S(1)}, bf16[512,640]{1,0:T(8,128)(2,1)S(1)}, u32[]{:S(2)}, u32[]{:S(2)}) collective-permute-start(bf16[512,640]{1,0:T(8,128)(2,1)S(1)} %slice.317), channel_id=1, source_target_pairs={{0,2},{1,3},{2,0},{3,1},{4,6},{5,7},{6,4},{7,5},{8,10},{9,11},{10,... | collective-permute-start | bytes 1966088 | tf_op jit(solution)/shard_map/ppermute | solution.py:38
  503.2 16.1 %collective-permute-start.29 = (bf16[512,640]{1,0:T(8,128)(2,1)S(1)}, bf16[512,640]{1,0:T(8,128)(2,1)S(1)}, u32[]{:S(2)}, u32[]{:S(2)}) collective-permute-start(bf16[512,640]{1,0:T(8,128)(2,1)S(1)} %slice.318), channel_id=1, source_target_pairs={{0,1},{1,0},{2,3},{3,2},{4,5},{5,4},{6,7},{7,6},{8,9},{9,8},{10,11... | collective-permute-start | bytes 1966088 | tf_op jit(solution)/shard_map/ppermute | solution.py:38
  533.7 3.7 collective-permute-start.46
  540.5 241.6 %reduce-scatter.11.cloned.1.call-start = ((), (), s32[]{:S(2)}) async-start(), calls=%async_computation.14 | async-start | bytes 8601600 | tf_op jit(solution)/shard_map/reduce_scatter | solution.py:583
  550.3 284.6 %reduce-scatter.9.cloned.1.call-start = ((), (), s32[]{:S(2)}) async-start(), calls=%async_computation.13 | async-start | bytes 9830400 | tf_op jit(solution)/shard_map/reduce_scatter | solution.py:583
  550.5 12.8 %collective-permute-start.47 = (bf16[1280,3072]{1,0:T(8,128)(2,1)}, bf16[1280,3072]{1,0:T(8,128)(2,1)}, u32[]{:S(2)}, u32[]{:S(2)}) collective-permute-start(bf16[1280,3072]{1,0:T(8,128)(2,1)} %get-tuple-element.91), channel_id=1, source_target_pairs={{0,4},{4,0},{8,12},{12,8},{16,20},{20,16},{24,28},{28,24},{1,5},{5... | collective-permute-start | bytes 23592968 | tf_op jit(solution)/shard_map/ppermute | solution.py:580
  575.6 21.6 %all-to-all-start.2 = ((bf16[4,256,640]{2,1,0:T(8,128)(2,1)}), bf16[4,256,640]{2,1,0:T(8,128)(2,1)}, u32[]{:S(2)}, u32[]{:S(2)}) async-start(bf16[4,256,640]{2,1,0:T(8,128)(2,1)} %bitcast.26), calls=%async_computation.2 | async-start | bytes 2621440 | tf_op jit(solution)/shard_map/all_to_all | solution.py:142
  615.2 7.6 collective-permute-start.30
  616.7 7.6 collective-permute-start.32
  622.8 5.0 collective-permute-start.31
  627.9 5.0 collective-permute-start.33
  636.2 37.8 %all-to-all-start.3 = ((bf16[256,4,768]{2,0,1:T(8,128)(2,1)}), bf16[256,4,768]{2,0,1:T(8,128)(2,1)}, u32[]{:S(2)}, u32[]{:S(2)}) async-start(bf16[256,4,768]{2,0,1:T(8,128)(2,1)} %bitcast.138), calls=%async_computation.3 | async-start | bytes 3145728 | tf_op jit(solution)/shard_map/all_to_all | solution.py:146
  640.6 239.2 %reduce-scatter.5.cloned.1.call-start = ((), (), s32[]{:S(2)}) async-start(), calls=%async_computation.11 | async-start | bytes 2457600 | tf_op jit(solution)/shard_map/reduce_scatter | solution.py:583
  670.6 27.9 %collective-permute-start.22 = (bf16[2,512,640]{2,1,0:T(8,128)(2,1)}, bf16[2,512,640]{2,1,0:T(8,128)(2,1)}, u32[]{:S(2)}, u32[]{:S(2)}) collective-permute-start(bf16[2,512,640]{2,1,0:T(8,128)(2,1)} %get-tuple-element.72), channel_id=1, source_target_pairs={{0,1},{1,0},{2,3},{3,2},{4,5},{5,4},{6,7},{7,6},{8,9},{9,8},{10,11... | collective-permute-start | bytes 3932168 | tf_op jit(solution)/shard_map/ppermute | solution.py:38
  672.6 30.9 %collective-permute-start.24 = (bf16[2,512,640]{2,1,0:T(8,128)(2,1)}, bf16[2,512,640]{2,1,0:T(8,128)(2,1)}, u32[]{:S(2)}, u32[]{:S(2)}) collective-permute-start(bf16[2,512,640]{2,1,0:T(8,128)(2,1)} %get-tuple-element.74), channel_id=1, source_target_pairs={{0,2},{1,3},{2,0},{3,1},{4,6},{5,7},{6,4},{7,5},{8,10},{9,11},{10,... | collective-permute-start | bytes 3932168 | tf_op jit(solution)/shard_map/ppermute | solution.py:38
  696.4 30.3 %collective-permute-start.45 = (bf16[1280,768]{1,0:T(8,128)(2,1)}, bf16[1280,768]{1,0:T(8,128)(2,1)}, u32[]{:S(2)}, u32[]{:S(2)}) collective-permute-start(bf16[1280,768]{1,0:T(8,128)(2,1)} %get-tuple-element.86), channel_id=1, source_target_pairs={{0,4},{4,0},{8,12},{12,8},{16,20},{20,16},{24,28},{28,24},{1,5},{5... | collective-permute-start | bytes 5898248 | tf_op jit(solution)/shard_map/ppermute | solution.py:580
  700.6 15.4 %collective-permute-start.23 = (bf16[512,640]{1,0:T(8,128)(2,1)}, bf16[512,640]{1,0:T(8,128)(2,1)}, u32[]{:S(2)}, u32[]{:S(2)}) collective-permute-start(bf16[512,640]{1,0:T(8,128)(2,1)} %fusion.37), channel_id=1, source_target_pairs={{0,2},{1,3},{2,0},{3,1},{4,6},{5,7},{6,4},{7,5},{8,10},{9,11},{10,... | collective-permute-start | bytes 1966088 | tf_op jit(solution)/shard_map/ppermute | solution.py:38
  706.1 24.0 %collective-permute-start.25 = (bf16[512,640]{1,0:T(8,128)(2,1)}, bf16[512,640]{1,0:T(8,128)(2,1)}, u32[]{:S(2)}, u32[]{:S(2)}) collective-permute-start(bf16[512,640]{1,0:T(8,128)(2,1)} %fusion.38), channel_id=1, source_target_pairs={{0,1},{1,0},{2,3},{3,2},{4,5},{5,4},{6,7},{7,6},{8,9},{9,8},{10,11... | collective-permute-start | bytes 1966088 | tf_op jit(solution)/shard_map/ppermute | solution.py:38
  708.6 10.6 %collective-permute-start.40 = (f32[8,320]{1,0:T(8,128)}, f32[8,320]{1,0:T(8,128)S(1)}, u32[]{:S(2)}, u32[]{:S(2)}) collective-permute-start(f32[8,320]{1,0:T(8,128)} %reshape.171), channel_id=1, source_target_pairs={{0,4},{4,0},{8,12},{12,8},{16,20},{20,16},{24,28},{28,24},{1,5},{5... | collective-permute-start | bytes 30728 | tf_op jit(solution)/shard_map/ppermute | solution.py:136
  718.7 31.6 %collective-permute-start.34 = (bf16[2,512,640]{2,1,0:T(8,128)(2,1)}, bf16[2,512,640]{2,1,0:T(8,128)(2,1)}, u32[]{:S(2)}, u32[]{:S(2)}) collective-permute-start(bf16[2,512,640]{2,1,0:T(8,128)(2,1)} %get-tuple-element.79), channel_id=1, source_target_pairs={{0,1},{1,0},{2,3},{3,2},{4,5},{5,4},{6,7},{7,6},{8,9},{9,8},{10,11... | collective-permute-start | bytes 3932168 | tf_op jit(solution)/shard_map/ppermute | solution.py:38
  719.2 5.4 collective-permute-start.41
  721.1 26.8 %collective-permute-start.38 = (f32[4,256]{1,0:T(4,128)S(1)}, f32[4,256]{1,0:T(4,128)S(1)}, u32[]{:S(2)}, u32[]{:S(2)}) collective-permute-start(f32[4,256]{1,0:T(4,128)S(1)} %dynamic_update_slice.65), channel_id=1, source_target_pairs={{0,1},{1,0},{2,3},{3,2},{4,5},{5,4},{6,7},{7,6},{8,9},{9,8},{10,11... | collective-permute-start | bytes 12296 | tf_op jit(solution)/shard_map/ppermute | solution.py:38
  724.6 32.0 %collective-permute-start.36 = (bf16[2,512,640]{2,1,0:T(8,128)(2,1)}, bf16[2,512,640]{2,1,0:T(8,128)(2,1)}, u32[]{:S(2)}, u32[]{:S(2)}) collective-permute-start(bf16[2,512,640]{2,1,0:T(8,128)(2,1)} %get-tuple-element.81), channel_id=1, source_target_pairs={{0,2},{1,3},{2,0},{3,1},{4,6},{5,7},{6,4},{7,5},{8,10},{9,11},{10,... | collective-permute-start | bytes 3932168 | tf_op jit(solution)/shard_map/ppermute | solution.py:38
  726.7 8.7 collective-permute-start.42
  735.4 14.4 %collective-permute-start.43 = (f32[8,320]{1,0:T(8,128)S(1)}, f32[8,320]{1,0:T(8,128)S(1)}, u32[]{:S(2)}, u32[]{:S(2)}) collective-permute-start(f32[8,320]{1,0:T(8,128)S(1)} %add.414), channel_id=1, source_target_pairs={{0,1},{1,0},{2,3},{3,2},{4,5},{5,4},{6,7},{7,6},{8,9},{9,8},{10,11... | collective-permute-start | bytes 30728 | tf_op jit(solution)/shard_map/ppermute | solution.py:38
  748.2 11.9 %collective-permute-start.39 = (f32[4,256]{1,0:T(4,128)S(1)}, f32[4,256]{1,0:T(4,128)S(1)}, u32[]{:S(2)}, u32[]{:S(2)}) collective-permute-start(f32[4,256]{1,0:T(4,128)S(1)} %add.409), channel_id=1, source_target_pairs={{0,2},{1,3},{2,0},{3,1},{4,6},{5,7},{6,4},{7,5},{8,10},{9,11},{10,... | collective-permute-start | bytes 12296 | tf_op jit(solution)/shard_map/ppermute | solution.py:38
  749.8 10.3 %collective-permute-start.44 = (f32[8,320]{1,0:T(8,128)S(1)}, f32[8,320]{1,0:T(8,128)S(1)}, u32[]{:S(2)}, u32[]{:S(2)}) collective-permute-start(f32[8,320]{1,0:T(8,128)S(1)} %add.415), channel_id=1, source_target_pairs={{0,2},{1,3},{2,0},{3,1},{4,6},{5,7},{6,4},{7,5},{8,10},{9,11},{10,... | collective-permute-start | bytes 30728 | tf_op jit(solution)/shard_map/ppermute | solution.py:38
  752.4 17.7 %collective-permute-start.35 = (bf16[512,640]{1,0:T(8,128)(2,1)}, bf16[512,640]{1,0:T(8,128)(2,1)S(1)}, u32[]{:S(2)}, u32[]{:S(2)}) collective-permute-start(bf16[512,640]{1,0:T(8,128)(2,1)} %fusion.39), channel_id=1, source_target_pairs={{0,2},{1,3},{2,0},{3,1},{4,6},{5,7},{6,4},{7,5},{8,10},{9,11},{10,... | collective-permute-start | bytes 1966088 | tf_op jit(solution)/shard_map/ppermute | solution.py:38
  758.7 15.4 %collective-permute-start.37 = (bf16[512,640]{1,0:T(8,128)(2,1)}, bf16[512,640]{1,0:T(8,128)(2,1)}, u32[]{:S(2)}, u32[]{:S(2)}) collective-permute-start(bf16[512,640]{1,0:T(8,128)(2,1)} %fusion.40), channel_id=1, source_target_pairs={{0,1},{1,0},{2,3},{3,2},{4,5},{5,4},{6,7},{7,6},{8,9},{9,8},{10,11... | collective-permute-start | bytes 1966088 | tf_op jit(solution)/shard_map/ppermute | solution.py:38
  840.4 41.6 %collective-permute-start.49 = (f32[320]{0:T(512)S(1)}, f32[320]{0:T(512)S(1)}, u32[]{:S(2)}, u32[]{:S(2)}) collective-permute-start(f32[320]{0:T(512)S(1)} %get-tuple-element.108), channel_id=1, source_target_pairs={{0,1},{1,0},{2,3},{3,2},{4,5},{5,4},{6,7},{7,6},{8,9},{9,8},{10,11... | collective-permute-start | bytes 3848 | tf_op jit(solution)/shard_map/ppermute | solution.py:38
  882.0 4.3 collective-permute-start.50
  (70 other events, 935.0 us)
Sparse Core Ops, SparseCore 0:
  11.4 74.9 all-gather.3
  88.6 141.0 all-gather.5
  232.0 124.5 all-gather.7
  540.6 33.2 reduce-scatter.6
  576.1 119.2 reduce-scatter.10
  697.5 137.2 reduce-scatter.8
  837.7 42.0 reduce-scatter.4

commit v7 on v6

--- a/solution.py
+++ b/solution.py
@@ -108,13 +108,15 @@
     return block, along_x, along_y, top, bottom
 
 
-def scatter_payload(payload):
+def scatter_payload(payload, *earlier):
     top_sent, bottom_sent, top_kept, bottom_kept = payload
     got_top = swap(top_sent, 1)
     got_bottom = swap(bottom_sent, 2)
     halves = []
     for kept, got, second in ((top_kept, got_top, 2), (bottom_kept, got_bottom, 1)):
         passed = (kept[1].astype(F32) + got[1].astype(F32)).astype(BF16)
+        if earlier:
+            passed = after(passed, *earlier)
         last = swap(passed, second)
         halves.append(kept[0].astype(F32) + got[0].astype(F32) + last.astype(F32))
     return jnp.concatenate(halves, axis=0)
@@ -144,6 +146,143 @@
 
 def cols_to_rows(block):
     return lax.all_to_all(block, "mdl", split_axis=1, concat_axis=0, tiled=True)
+
+
+def first_kernel(
+    x_ref, w_ref, rows_ref, weight_ref, own, x_sent, x_got, w_up, w_down, w_core, w_got
+):
+    me, tok = lax.axis_index("mdl"), lax.axis_index("tok")
+    pairs = lax.axis_size("tok") // 2
+    level, last = tok // 2, pairs - 1
+    half, width, shard = x_ref.shape[0] // 2, x_ref.shape[1], w_ref.shape[0]
+    below, above = level > 0, level < last
+
+    barrier = pltpu.get_barrier_semaphore()
+    pl.semaphore_signal(barrier, inc=1, device_id={"mdl": me ^ 1})
+    pl.semaphore_signal(barrier, inc=1, device_id={"mdl": me ^ 2})
+    pl.semaphore_signal(barrier, inc=1, device_id={"tok": tok ^ 1})
+
+    @pl.when(below)
+    def _():
+        pl.semaphore_signal(barrier, inc=1, device_id={"tok": tok - 2})
+
+    @pl.when(above)
+    def _():
+        pl.semaphore_signal(barrier, inc=1, device_id={"tok": tok + 2})
+
+    pl.semaphore_wait(barrier, 3 + below.astype(jnp.int32) + above.astype(jnp.int32))
+
+    def cols(block):
+        return pl.ds(pl.multiple_of(block * width, 128), width)
+
+    def block(index):
+        return weight_ref.at[pl.ds(pl.multiple_of(index * shard, 16), shard)]
+
+    def x_copy(source, target, at, to):
+        return pltpu.make_async_remote_copy(
+            source, target, x_sent.at[at], x_got.at[at], device_id={"mdl": me ^ to}
+        )
+
+    def w_copy(source, index, sent, to):
+        return pltpu.make_async_remote_copy(
+            source, block(index), sent, w_got.at[index], device_id={"tok": to}
+        )
+
+    mine = rows_ref.at[:, cols(me)]
+    to_x, to_y = x_copy(x_ref, mine, 0, 1), x_copy(x_ref, mine, 1, 2)
+
+    @pl.when(above)
+    def _():
+        w_copy(w_ref, tok, w_up.at[0], tok + 2).start()
+
+    @pl.when(below)
+    def _():
+        w_copy(w_ref, tok, w_down.at[0], tok - 2).start()
+
+    to_x.start()
+    to_y.start()
+    w_copy(w_ref, tok, w_core.at[tok], tok ^ 1).start()
+    keep_x = pltpu.make_async_copy(x_ref, mine, own.at[0])
+    keep_w = pltpu.make_async_copy(w_ref, block(tok), own.at[1])
+    keep_x.start()
+    keep_w.start()
+
+    def relay(distance):
+        low, high = tok - 2 * distance, tok + 2 * distance
+
+        @pl.when(level >= distance)
+        def _():
+            w_copy(block(low), low, w_core.at[low], tok ^ 1).wait_recv()
+
+            @pl.when(above)
+            def _():
+                w_copy(block(low), low, w_up.at[distance], tok + 2).start()
+
+            w_copy(block(low), low, w_core.at[low], tok ^ 1).start()
+
+        @pl.when(level + distance <= last)
+        def _():
+            w_copy(block(high), high, w_core.at[high], tok ^ 1).wait_recv()
+
+            @pl.when(below)
+            def _():
+                w_copy(block(high), high, w_down.at[distance], tok - 2).start()
+
+            w_copy(block(high), high, w_core.at[high], tok ^ 1).start()
+
+    relay(1)
+    from_x = rows_ref.at[pl.ds(0, half), cols(me ^ 1)]
+    from_y = rows_ref.at[pl.ds(half, half), cols(me ^ 2)]
+    top, bottom = x_copy(from_x, from_x, 2, 2), x_copy(from_y, from_y, 3, 1)
+    to_x.wait_recv()
+    top.start()
+    to_y.wait_recv()
+    bottom.start()
+    for distance in range(2, pairs):
+        relay(distance)
+    for copy in (keep_x, keep_w):
+        copy.wait()
+    for copy in (top, bottom):
+        copy.wait_recv()
+    for copy in (to_x, to_y, top, bottom):
+        copy.wait_send()
+
+    for distance in range(pairs):
+
+        @pl.when((level >= distance) & above)
+        def _(distance=distance):
+            w_copy(block(tok), tok, w_up.at[distance], tok + 2).wait_send()
+
+        @pl.when((level + distance <= last) & below)
+        def _(distance=distance):
+            w_copy(block(tok), tok, w_down.at[distance], tok - 2).wait_send()
+
+        near, far = 2 * distance + tok % 2, 2 * distance + 1 - tok % 2
+        w_copy(block(near), near, w_core.at[near], tok ^ 1).wait_send()
+        w_copy(block(far), far, w_core.at[near], tok ^ 1).wait_recv()
+
+
+def first_gather(inputs, weight):
+    tokens, width = inputs.shape
+    shard, cols = weight.shape
+    pairs = lax.axis_size("tok") // 2
+    dma = pltpu.SemaphoreType.DMA
+    return pl.pallas_call(
+        first_kernel,
+        out_shape=(
+            jax.ShapeDtypeStruct((tokens, 4 * width), BF16),
+            jax.ShapeDtypeStruct((2 * pairs * shard, cols), BF16),
+        ),
+        in_specs=[pl.BlockSpec(memory_space=pltpu.VMEM)] * 2,
+        out_specs=[pl.BlockSpec(memory_space=pl.ANY)] * 2,
+        scratch_shapes=[
+            dma((2,)), dma((4,)), dma((4,)), dma((pairs,)), dma((pairs,)),
+            dma((2 * pairs,)), dma((2 * pairs,)),
+        ],
+        compiler_params=pltpu.CompilerParams(
+            collective_id=0, has_side_effects=True, vmem_limit_bytes=16 << 20
+        ),
+    )(inputs, weight)
 
 
 def in_order(mebibytes):
@@ -534,9 +673,9 @@
 def product_to_mdl(lefts, weight, starts, partial=()):
     if lax.axis_size("mdl") == 4:
         payload = scatter_product(lefts, weight, starts, partial)
-        return payload, lambda payload: scatter_payload(payload)
+        return payload, lambda payload, *earlier: scatter_payload(payload, *earlier)
     part = sum((sum_products(lefts, weight, starts), *partial))
-    return (part.astype(BF16),), lambda payload: scatter_mdl(payload[0], 1)
+    return (part.astype(BF16),), lambda payload, *earlier: scatter_mdl(payload[0], 1)
 
 
 def after(value, *earlier):
@@ -587,17 +726,23 @@
 
     qkv_cols, ff_cols = qkv_weight.shape[1], gate_weight.shape[1]
     attn_local = jnp.concatenate([scaled(qkv_weight, norm1_gain), out_weight.T], axis=1)
-    w_attn = from_tok(attn_local, 0)
-    w_qkv = w_attn[:, :qkv_cols]
     middle = -(-ff_cols // 256) * 128
     parts = ((0, middle), (middle, ff_cols))
-    w_parts = []
-    for start, stop in parts:
+
+    def part_local(start, stop):
         local = [scaled(w[:, start:stop], norm2_gain) for w in (gate_weight, up_weight)]
-        local = jnp.concatenate([*local, down_weight[start:stop].T], axis=1)
-        w_parts.append(from_tok(local, 0))
-
-    rows_in = gather_mdl(inputs, 1)
+        return jnp.concatenate([*local, down_weight[start:stop].T], axis=1)
+
+    locals_ff = [part_local(*part) for part in parts]
+    if size == 4 and lax.axis_size("tok") == 8:
+        rows_in, w_attn = first_gather(inputs, after(attn_local, locals_ff[0]))
+        locals_ff = lax.optimization_barrier((*locals_ff, w_attn))[:-1]
+    else:
+        rows_in = gather_mdl(inputs, 1)
+        w_attn = from_tok(attn_local, 0)
+    w_qkv = w_attn[:, :qkv_cols]
+    w_parts = [from_tok(local, 0) for local in locals_ff]
+
     scale_one = row_scale(rows_in)
     qkv_part = (nn(rows_in, w_qkv) * scale_one).astype(BF16)
     qkv = rows_to_cols(qkv_part)
@@ -682,7 +827,7 @@
     *qkv_local, gain_one = pair_grad(rows_in, d_scaled, w_attn)
     qkv_sum = pair_to_tok(qkv_local)
     d_one = scatter(payload)
-    ffn_sum = ffn_scatter(ffn_payload)
+    ffn_sum = ffn_scatter(ffn_payload, d_qkv_part)
     block_out = (mixed + ffn_sum).astype(BF16)
     input_grad = d_mixed + scale_one * (d_one - (scale_one * residual) * stat_one)
 

time: 903 us -> 904 us (level)
  waiting for transfers between devices: 407 us -> 333 us
  Pallas kernels: 178 us -> 246 us
    pallas_call x0 -> x1, Pallas kernels: none -> 67.5 us  [first_gather(): pl.pallas_call(first_kernel, out_shape=(jax.ShapeDtypeStruct((tokens, 4 *...]
    ppermute x44 -> x40, waiting for transfers between devices: 240 us -> 214 us  [swap(): return lax.ppermute(block, 'mdl', [(i, i ^ distance) for i in range(size)])]
    reduce_scatter x4, waiting for transfers between devices: 87.6 us -> 61.3 us  [pair_to_tok(): lax.psum_scatter(both, 'tok', scatter_dimension=0, tiled=True, axis_index...]
    all_gather x3 -> x2, waiting for transfers between devices: 21.7 us -> 0.01 us  [from_tok(): return lax.all_gather(weight, 'tok', axis=dim, tiled=True)]
    ppermute x44 -> x40, starting transfers between devices: 54.9 us -> 47.4 us  [swap(): return lax.ppermute(block, 'mdl', [(i, i ^ distance) for i in range(size)])]
    unnamed x147 -> x143, local copies, waits for them, and re-layouts: 14.2 us -> 21.2 us
  transfers between devices with their start and end apart: 61 -> 56, of which waited for: 35 -> 26; matrix products, arithmetic and copies ran while one was open for 18% -> 18% of each run, Pallas kernels for 18% -> 18%
where the time goes in v7:
time: 904 us; the launch traced here: 897 us
  waiting for transfers between devices  333 us (37%)
  Pallas kernels  246 us (27%)
  other arithmetic  102 us (11%)
  matrix products  68.9 us (8%)
  starting transfers between devices  61.3 us (7%)
  local copies, waits for them, and re-layouts  51.1 us (6%)
  blocking collectives  18.7 us (2%)
  between operations  15.4 us (2%)
    ppermute x40, waiting for transfers between devices, swap(): return lax.ppermute(block, 'mdl', [(i, i ^ distance) for i in range(size)])  214 us
    dot_general x7, matrix products, nn(): return jnp.dot(left_op, right_op, preferred_element_type=F32)  68.9 us
    pallas_call x1, Pallas kernels, first_gather(): pl.pallas_call(first_kernel, out_shape=(jax.ShapeDtypeStruct((tokens, 4 *...  67.5 us
    reduce_scatter x4, waiting for transfers between devices, pair_to_tok(): lax.psum_scatter(both, 'tok', scatter_dimension=0, tiled=True, axis_index...  61.3 us
    pallas_call x2, Pallas kernels, part_grad(): pl.pallas_call(part_kernel, grid=(pairs,), out_shape=(out, out), in_specs...  48.3 us
    pallas_call x4, Pallas kernels, scatter_product(): pl.pallas_call(functools.partial(payload_kernel, starts), grid_spec=pltpu...  48.3 us
    ppermute x40, starting transfers between devices, swap(): return lax.ppermute(block, 'mdl', [(i, i ^ distance) for i in range(size)])  47.4 us
    all_to_all x2, waiting for transfers between devices, rows_to_cols(): return lax.all_to_all(block, 'mdl', split_axis=0, concat_axis=1, tiled=True)  36.8 us
  transfers between devices with their start and end apart: 56, of which 26 were waited for; matrix products, arithmetic and copies ran while one was open for 18% of the time, Pallas kernels for 18%

profile of v7, /device:TPU:0, one launch (start us, length us, event | category | flops | bytes accessed | tf_op | source)
XLA Modules:
  0.0 896.7 jit_solution(14024995376670591470)
XLA Ops:
  14.0 67.5 %shard_map.169 = (bf16[1024,2560]{1,0:T(8,128)(2,1)S(1)}, bf16[2560,1408]{1,0:T(8,128)(2,1)S(1)}) custom-call(bf16[1024,640]{1,0:T(8,128)(2,1)S(1)} %copy-done, bf16[320,1408]{1,0:T(8,128)(2,1)S(1)} %pad_maximum_fusion.5.w_ref), custom_call_target="tpu_custom_call" | custom-call | tf_op jit(solution)/shard_map/pallas_call | solution.py:270
  81.6 3.0 copy-done.1
  89.0 3.7 multiply_reduce_fusion
  93.0 7.9 multiply_convert_fusion.3
  101.0 4.1 all-to-all-start
  105.1 19.8 %all-to-all-done = bf16[4,256,768]{2,1,0:T(8,128)(2,1)S(1)} async-done(((bf16[4,256,768]{2,1,0:T(8,128)(2,1)}), bf16[4,256,768]{2,1,0:T(8,128)(2,1)S(1)}, u32[]{:S(2)}, u32[]{:S(2)}) %all-to-all-start) | async-done | bytes 1572896 | tf_op jit(solution)/shard_map/all_to_all | solution.py:144
  132.3 5.7 collective-permute-done
  146.1 12.0 %attention_forward.1 = (bf16[256,2560]{1,0:T(8,128)(2,1)S(1)}, f32[10,256,1]{2,1,0:T(8,128)S(1)}) custom-call(s32[1]{0:T(128)} %bitcast.1.first_ref, bf16[256,3072]{1,0:T(8,128)(2,1)S(1)} %bitcast.131, bf16[1024,512]{1,0:T(8,128)(2,1)} %constant_dynamic-update-slice_fusion.4.kv_ref, f32[256,128]{1,0:T(8,128)S(1)} %get-tuple-element.151.cos_ref, ...), custom_call_target="tpu_custom_call" | custom-call | flops 2684354560 | bytes 3670016 | tf_op jit(solution)/shard_map/attention_forward/pallas_call | solution.py:364
  158.3 18.7 %all_to_all.76 = bf16[256,4,640]{2,0,1:T(8,128)(2,1)} all-to-all(bf16[256,4,640]{2,0,1:T(8,128)(2,1)S(1)} %bitcast.141), channel_id=1, replica_groups=mesh['tok'=8,'mdl'=4] {'mdl'}, dimensions={1} | all-to-all | bytes 2621440 | tf_op jit(solution)/shard_map/all_to_all | solution.py:148
  177.0 7.8 shard_map.170
  186.6 25.6 %collective-permute-done.4 = bf16[2,512,640]{2,1,0:T(8,128)(2,1)S(1)} collective-permute-done((bf16[2,512,640]{2,1,0:T(8,128)(2,1)S(1)}, bf16[2,512,640]{2,1,0:T(8,128)(2,1)S(1)}, u32[]{:S(2)}, u32[]{:S(2)}) %collective-permute-start.4) | collective-permute-done | bytes 1310752 | tf_op jit(solution)/shard_map/ppermute | solution.py:38
  216.4 10.9 %collective-permute-done.5 = bf16[512,640]{1,0:T(8,128)(2,1)} collective-permute-done((bf16[512,640]{1,0:T(8,128)(2,1)}, bf16[512,640]{1,0:T(8,128)(2,1)}, u32[]{:S(2)}, u32[]{:S(2)}) %collective-permute-start.5) | collective-permute-done | bytes 655392 | tf_op jit(solution)/shard_map/ppermute | solution.py:38
  230.9 2.7 broadcast_in_dim.12
  237.2 24.9 %collective-permute-done.8 = bf16[1024,640]{1,0:T(8,128)(2,1)S(1)} collective-permute-done((bf16[1024,640]{1,0:T(8,128)(2,1)S(1)}, bf16[1024,640]{1,0:T(8,128)(2,1)S(1)}, u32[]{:S(2)}, u32[]{:S(2)}) %collective-permute-start.8) | collective-permute-done | bytes 1310752 | tf_op jit(solution)/shard_map/ppermute | solution.py:38
  268.2 2.7 constant_dynamic-update-slice_fusion.2
  272.2 4.3 collective-permute-done.10
  280.8 3.7 fusion
  284.5 5.8 fusion.1.rows_ref
  290.3 9.6 %fusion.2 = f32[1024,1024]{1,0:T(8,128)S(1)} fusion(bf16[1024,2560]{1,0:T(8,128)(2,1)} %fusion.1.rows_ref, bf16[2560,3072]{1,0:T(8,128)(2,1)} %all-gather.3.cloned.1.call-done.refs_2_.refs_1_), kind=kOutput, calls=%fused_computation.7 | convolution fusion | flops 5368709120 | bytes 14680064 | tf_op jit(solution)/shard_map/dot_general | solution.py:33
  299.9 9.2 %fusion.6 = f32[1024,1024]{0,1:T(8,128)S(1)} fusion(bf16[1024,2560]{1,0:T(8,128)(2,1)} %above_ref.2, bf16[2560,3072]{1,0:T(8,128)(2,1)} %all-gather.3.cloned.1.call-done.refs_2_.refs_1_), kind=kOutput, calls=%fused_computation.11 | convolution fusion | flops 5368709120 | bytes 14680064 | tf_op jit(solution)/shard_map/dot_general | solution.py:33
  309.2 11.7 %add_reduce_fusion = (f32[1024]{0:T(1024)S(1)}, bf16[1024,1024]{1,0:T(8,128)(2,1)S(1)}, bf16[1024,1024]{1,0:T(8,128)(2,1)S(1)}, bf16[1024,1024]{1,0:T(8,128)(2,1)}) fusion(f32[1024,1024]{1,0:T(8,128)S(1)} %fusion.2, f32[1024,1024]{0,1:T(8,128)S(1)} %fusion.6, bf16[1024,2560]{1,0:T(8,128)(2,1)S(1)} %bitcast.140, ...), kind=kOutput, calls=%fused_computation.22 | convolution fusion | flops 5398068224 | bytes 25169920 | tf_op jit(solution)/shard_map/dot_general | solution.py:33
  320.9 24.6 %shard_map.171 = (bf16[1280,3072]{1,0:T(8,128)(2,1)}, bf16[1280,3072]{1,0:T(8,128)(2,1)}) custom-call(s32[1]{0:T(128)} %bitcast.13.core_ref, bf16[1024,2560]{1,0:T(8,128)(2,1)} %fusion.1.rows_ref, bf16[1024,2560]{1,0:T(8,128)(2,1)} %above_ref.2, bf16[1024,1024]{1,0:T(8,128)(2,1)S(1)} %get-tuple-element.72.d_gate_ref.refs_0_, ...), custom_call_target="tpu_custom_call" | custom-call | flops 16106127360 | bytes 32505856 | tf_op jit(solution)/shard_map/pallas_call | solution.py:502
  345.5 15.8 %shard_map.172.refs_3_ = f32[1024,2560]{1,0:T(8,128)} custom-call(bf16[1024,1024]{1,0:T(8,128)(2,1)S(1)} %get-tuple-element.72.d_gate_ref.refs_0_, bf16[1024,1024]{1,0:T(8,128)(2,1)S(1)} %get-tuple-element.117.d_up_ref.refs_1_, bf16[2560,3072]{1,0:T(8,128)(2,1)} %all-gather.3.cloned.1.call-done.refs_2_.refs_1_), custom_call_target="tpu_custom_call" | custom-call | flops 10737418240 | bytes 26214400 | tf_op jit(solution)/shard_map/pallas_call | solution.py:574
  361.4 8.8 fusion.10
  370.2 8.9 fusion.8
  379.1 12.8 %fusion.67 = (bf16[1024,896]{1,0:T(8,128)(2,1)}, f32[1024]{0:T(1024)S(1)}, bf16[1024,896]{1,0:T(8,128)(2,1)}, bf16[1024,896]{1,0:T(8,128)(2,1)S(1)}) fusion(f32[1024,896]{1,0:T(8,128)S(1)} %fusion.8, f32[1024,896]{1,0:T(8,128)S(1)} %fusion.10, bf16[1024,2560]{1,0:T(8,128)(2,1)} %fusion.1.rows_ref, ...), kind=kOutput, calls=%fused_computation.168 | convolution fusion | flops 4723309568 | bytes 22679552 | tf_op jit(solution)/shard_map/dot_general | solution.py:33
  391.8 18.4 %shard_map.173 = (bf16[2,512,640]{2,1,0:T(8,128)(2,1)S(1)}, bf16[2,512,640]{2,1,0:T(8,128)(2,1)S(1)}, bf16[2,512,640]{2,1,0:T(8,128)(2,1)S(1)}, bf16[2,512,640]{2,1,0:T(8,128)(2,1)S(1)}) custom-call(s32[1]{0:T(128)} %bitcast.me_ref, bf16[1024,896]{1,0:T(8,128)(2,1)} %get-tuple-element.115.refs_0_.d_gate_ref, ...), custom_call_target="tpu_custom_call" | custom-call | flops 9395240960 | bytes 22675456 | tf_op jit(solution)/shard_map/pallas_call | solution.py:615
  413.8 22.4 %collective-permute-done.16 = f32[8,128]{1,0:T(8,128)S(1)} collective-permute-done((f32[8,128]{1,0:T(8,128)S(1)}, f32[8,128]{1,0:T(8,128)S(1)}, u32[]{:S(2)}, u32[]{:S(2)}) %collective-permute-start.16) | collective-permute-done | bytes 4128 | tf_op jit(solution)/shard_map/ppermute | solution.py:38
  442.3 23.7 %shard_map.174 = (bf16[1280,2688]{1,0:T(8,128)(2,1)}, bf16[1280,2688]{1,0:T(8,128)(2,1)}) custom-call(s32[1]{0:T(128)} %bitcast.13.core_ref, bf16[1024,2560]{1,0:T(8,128)(2,1)} %fusion.1.rows_ref, bf16[1024,2560]{1,0:T(8,128)(2,1)} %above_ref.2, bf16[1024,896]{1,0:T(8,128)(2,1)S(1)} %copy-done.24, bf16[1024,896]{1,0:T(8,128)(2,1)S(1)} %copy-done.25, ...), custom_call_target="tpu_custom_call" | custom-call | flops 14092861440 | bytes 29753344 | tf_op jit(solution)/shard_map/pallas_call | solution.py:502
  468.1 4.1 fusion.68
  476.1 27.0 %collective-permute-done.19.along_x = bf16[1024,640]{1,0:T(8,128)(2,1)S(1)} collective-permute-done((bf16[1024,640]{1,0:T(8,128)(2,1)S(1)}, bf16[1024,640]{1,0:T(8,128)(2,1)S(1)}, u32[]{:S(2)}, u32[]{:S(2)}) %collective-permute-start.19) | collective-permute-done | bytes 1310752 | tf_op jit(solution)/shard_map/ppermute | solution.py:38
  503.1 2.5 collective-permute-start.21
  507.3 12.7 %collective-permute-done.21.top = bf16[512,640]{1,0:T(8,128)(2,1)S(1)} collective-permute-done((bf16[512,640]{1,0:T(8,128)(2,1)S(1)}, bf16[512,640]{1,0:T(8,128)(2,1)S(1)}, u32[]{:S(2)}, u32[]{:S(2)}) %collective-permute-start.21) | collective-permute-done | bytes 655392 | tf_op jit(solution)/shard_map/ppermute | solution.py:38
  521.5 6.8 shard_map.177
  528.3 7.6 shard_map.180
  535.9 3.7 collective-permute-done.42
  539.6 3.0 add_convert_fusion.3
  542.8 9.7 %add_convert_fusion.1 = bf16[1280,2688]{1,0:T(8,128)(2,1)} fusion(bf16[1280,2688]{1,0:T(8,128)(2,1)} %collective-permute-done.44, bf16[1280,2688]{1,0:T(8,128)(2,1)} %get-tuple-element.79), kind=kLoop, calls=%fused_computation.1 | loop fusion | flops 13762560 | bytes 20643840 | tf_op jit(solution)/shard_map/convert_element_type | solution.py:720
  552.9 12.6 %collective-permute-done.43 = bf16[1280,3072]{1,0:T(8,128)(2,1)} collective-permute-done((bf16[1280,3072]{1,0:T(8,128)(2,1)}, bf16[1280,3072]{1,0:T(8,128)(2,1)}, u32[]{:S(2)}, u32[]{:S(2)}) %collective-permute-start.43) | collective-permute-done | bytes 7864352 | tf_op jit(solution)/shard_map/ppermute | solution.py:719
  565.5 12.3 %add_convert_fusion = bf16[1280,3072]{1,0:T(8,128)(2,1)} fusion(bf16[1280,3072]{1,0:T(8,128)(2,1)} %collective-permute-done.43, bf16[1280,3072]{1,0:T(8,128)(2,1)} %get-tuple-element.68), kind=kLoop, calls=%fused_computation | loop fusion | flops 15728640 | bytes 23592960 | tf_op jit(solution)/shard_map/convert_element_type | solution.py:720
  577.8 4.3 all-to-all-start.2
  582.2 17.1 %all-to-all-done.2 = bf16[4,256,640]{2,1,0:T(8,128)(2,1)} async-done(((bf16[4,256,640]{2,1,0:T(8,128)(2,1)}), bf16[4,256,640]{2,1,0:T(8,128)(2,1)}, u32[]{:S(2)}, u32[]{:S(2)}) %all-to-all-start.2) | async-done | bytes 1310752 | tf_op jit(solution)/shard_map/all_to_all | solution.py:144
  601.4 16.8 %attention_backward.1 = (bf16[256,2560]{1,0:T(8,128)(2,1)S(1)}, f32[1024,512]{1,0:T(8,128)S(1)}) custom-call(s32[1]{0:T(128)} %bitcast.1.first_ref, bf16[256,3072]{1,0:T(8,128)(2,1)S(1)} %bitcast.132, bf16[1024,512]{1,0:T(8,128)(2,1)} %constant_dynamic-update-slice_fusion.4.kv_ref, f32[256,128]{1,0:T(8,128)S(1)} %get-tuple-element.151.cos_ref, ...), custom_call_target="tpu_custom_call" | custom-call | flops 6710886400 | bytes 8388608 | tf_op jit(solution)/shard_map/attention_backward/pallas_call | solution.py:389
  620.7 5.3 collective-permute-done.23
  628.2 3.7 collective-permute-done.24
  635.0 3.8 collective-permute-done.26
  643.0 4.3 all-to-all-start.3
  647.6 14.0 %shard_map.175.refs_2_ = f32[1024,2560]{1,0:T(8,128)} custom-call(bf16[1024,1024]{1,0:T(8,128)(2,1)S(1)} %copy-done.4, bf16[2560,3072]{1,0:T(8,128)(2,1)} %all-gather.3.cloned.1.call-done.refs_2_.refs_1_), custom_call_target="tpu_custom_call" | custom-call | flops 5368709120 | bytes 26214400 | tf_op jit(solution)/shard_map/pallas_call | solution.py:574
  661.6 13.6 %shard_map.176 = (bf16[2,512,640]{2,1,0:T(8,128)(2,1)}, bf16[2,512,640]{2,1,0:T(8,128)(2,1)}, bf16[2,512,640]{2,1,0:T(8,128)(2,1)S(1)}, bf16[2,512,640]{2,1,0:T(8,128)(2,1)S(1)}) custom-call(s32[1]{0:T(128)} %bitcast.me_ref, bf16[1024,896]{1,0:T(8,128)(2,1)} %copy-done.5, bf16[2560,2688]{1,0:T(8,128)(2,1)} %all-gather.5.cloned.1.call-done.refs_2_.refs_1_, ...), custom_call_target="tpu_custom_call" | custom-call | flops 4697620480 | bytes 20840448 | tf_op jit(solution)/shard_map/pallas_call | solution.py:615
  679.4 8.3 shard_map.178
  693.1 9.1 %shard_map.179 = (bf16[1280,768]{1,0:T(8,128)(2,1)S(1)}, bf16[1280,768]{1,0:T(8,128)(2,1)}, f32[2560,1]{1,0:T(8,128)S(1)}) custom-call(s32[1]{0:T(128)} %bitcast.13.core_ref, bf16[1024,2560]{1,0:T(8,128)(2,1)} %copy-done.2, bf16[1024,768]{1,0:T(8,128)(2,1)S(1)} %multiply_convert_fusion.2.right_ref, bf16[2560,1408]{1,0:T(8,128)(2,1)} %copy-done.1), custom_call_target="tpu_custom_call" | custom-call | flops 4026531840 | bytes 10747904 | tf_op jit(solution)/shard_map/pallas_call | solution.py:469
  706.9 3.2 fusion.37
  712.6 4.4 collective-permute-done.37
  716.9 17.9 %collective-permute-done.28 = bf16[2,512,640]{2,1,0:T(8,128)(2,1)} collective-permute-done((bf16[2,512,640]{2,1,0:T(8,128)(2,1)}, bf16[2,512,640]{2,1,0:T(8,128)(2,1)}, u32[]{:S(2)}, u32[]{:S(2)}) %collective-permute-start.28) | collective-permute-done | bytes 1310752 | tf_op jit(solution)/shard_map/ppermute | solution.py:38
  741.6 26.4 %collective-permute-done.39 = f32[8,320]{1,0:T(8,128)S(1)} collective-permute-done((f32[8,320]{1,0:T(8,128)S(1)}, f32[8,320]{1,0:T(8,128)S(1)}, u32[]{:S(2)}, u32[]{:S(2)}) %collective-permute-start.39) | collective-permute-done | bytes 10272 | tf_op jit(solution)/shard_map/ppermute | solution.py:38
  769.4 3.3 add_convert_fusion.2
  780.6 10.2 %collective-permute-done.27 = bf16[512,640]{1,0:T(8,128)(2,1)} collective-permute-done((bf16[512,640]{1,0:T(8,128)(2,1)}, bf16[512,640]{1,0:T(8,128)(2,1)}, u32[]{:S(2)}, u32[]{:S(2)}) %collective-permute-start.27) | collective-permute-done | bytes 655392 | tf_op jit(solution)/shard_map/ppermute | solution.py:38
  793.9 8.5 collective-permute-done.31
  805.9 3.1 fusion.22
  810.9 3.2 fusion.72
  814.2 23.6 %reduce-scatter.9.cloned.1.call-done = bf16[320,3072]{1,0:T(8,128)(2,1)} async-done(((bf16[1280,3072]{1,0:T(8,128)(2,1)}), bf16[320,3072]{1,0:T(8,128)(2,1)}) %reduce-scatter.9.cloned.1.call-update) | async-done | bytes 1966096 | tf_op jit(solution)/shard_map/reduce_scatter | solution.py:722
  840.3 3.0 fusion.26
  844.7 37.7 %reduce-scatter.5.cloned.1.call-done = bf16[320,768]{1,0:T(8,128)(2,1)} async-done(((bf16[1280,768]{1,0:T(8,128)(2,1)}), bf16[320,768]{1,0:T(8,128)(2,1)}) %reduce-scatter.5.cloned.1.call-update) | async-done | bytes 491536 | tf_op jit(solution)/shard_map/reduce_scatter | solution.py:722
  886.1 2.9 maximum_bitcast_fusion
  (324 shorter events, 134.9 us)
Async XLA Ops:
  7.2 283.1 %all-gather.3.cloned.1.call-start = ((), (), s32[]{:S(2)}) async-start(), calls=%async_computation.8 | async-start | bytes 17694720 | tf_op jit(solution)/shard_map/all_gather | solution.py:714
  14.0 72.9 %copy-start.46 = (bf16[320,896]{1,0:T(8,128)(2,1)S(1)}, bf16[320,896]{1,0:T(8,128)(2,1)}, u32[]{:S(2)}) copy-start(bf16[320,896]{1,0:T(8,128)(2,1)} %slice_bitcast_fusion.1) | copy-start | bytes 1720324
  88.2 273.1 %all-gather.5.cloned.1.call-start = ((), (), s32[]{:S(2)}) async-start(), calls=%async_computation.9 | async-start | bytes 15482880 | tf_op jit(solution)/shard_map/all_gather | solution.py:714
  101.0 23.9 %all-to-all-start = ((bf16[4,256,768]{2,1,0:T(8,128)(2,1)}), bf16[4,256,768]{2,1,0:T(8,128)(2,1)S(1)}, u32[]{:S(2)}, u32[]{:S(2)}) async-start(bf16[4,256,768]{2,1,0:T(8,128)(2,1)} %bitcast.142), calls=%async_computation | async-start | bytes 3145728 | tf_op jit(solution)/shard_map/all_to_all | solution.py:144
  105.1 703.9 %reduce-scatter.7.cloned.1.call-start = ((), (), s32[]{:S(2)}) async-start(), calls=%async_computation.11 | async-start | bytes 2048000 | tf_op jit(solution)/shard_map/reduce_scatter | solution.py:722
  130.2 7.8 collective-permute-start
  131.7 7.9 collective-permute-start.1
  138.0 5.4 collective-permute-start.2
  140.5 5.0 collective-permute-start.3
  184.9 29.7 %copy-start.19 = (bf16[2,512,640]{2,1,0:T(8,128)(2,1)}, bf16[2,512,640]{2,1,0:T(8,128)(2,1)S(1)}, u32[]{:S(2)}) copy-start(bf16[2,512,640]{2,1,0:T(8,128)(2,1)S(1)} %get-tuple-element.65) | copy-start | bytes 3932164
  184.9 30.8 %copy-start.21 = (bf16[2,512,640]{2,1,0:T(8,128)(2,1)}, bf16[2,512,640]{2,1,0:T(8,128)(2,1)S(1)}, u32[]{:S(2)}) copy-start(bf16[2,512,640]{2,1,0:T(8,128)(2,1)S(1)} %get-tuple-element.63) | copy-start | bytes 3932164
  184.9 27.2 %collective-permute-start.4 = (bf16[2,512,640]{2,1,0:T(8,128)(2,1)S(1)}, bf16[2,512,640]{2,1,0:T(8,128)(2,1)S(1)}, u32[]{:S(2)}, u32[]{:S(2)}) collective-permute-start(bf16[2,512,640]{2,1,0:T(8,128)(2,1)S(1)} %get-tuple-element.64), channel_id=1, source_target_pairs={{0,1},{1,0},{2,3},{3,2},{4,5},{5,4},{6,7},{7,6},{8,9},{9,8},{10,11... | collective-permute-start | bytes 3932168 | tf_op jit(solution)/shard_map/ppermute | solution.py:38
  185.9 28.7 %collective-permute-start.6 = (bf16[2,512,640]{2,1,0:T(8,128)(2,1)S(1)}, bf16[2,512,640]{2,1,0:T(8,128)(2,1)S(1)}, u32[]{:S(2)}, u32[]{:S(2)}) collective-permute-start(bf16[2,512,640]{2,1,0:T(8,128)(2,1)S(1)} %get-tuple-element.66), channel_id=1, source_target_pairs={{0,2},{1,3},{2,0},{3,1},{4,6},{5,7},{6,4},{7,5},{8,10},{9,11},{10,... | collective-permute-start | bytes 3932168 | tf_op jit(solution)/shard_map/ppermute | solution.py:38
  213.3 14.0 %collective-permute-start.5 = (bf16[512,640]{1,0:T(8,128)(2,1)}, bf16[512,640]{1,0:T(8,128)(2,1)}, u32[]{:S(2)}, u32[]{:S(2)}) collective-permute-start(bf16[512,640]{1,0:T(8,128)(2,1)} %fusion.33), channel_id=1, source_target_pairs={{0,2},{1,3},{2,0},{3,1},{4,6},{5,7},{6,4},{7,5},{8,10},{9,11},{10,... | collective-permute-start | bytes 1966088 | tf_op jit(solution)/shard_map/ppermute | solution.py:38
  215.9 13.1 %collective-permute-start.7 = (bf16[512,640]{1,0:T(8,128)(2,1)}, bf16[512,640]{1,0:T(8,128)(2,1)}, u32[]{:S(2)}, u32[]{:S(2)}) collective-permute-start(bf16[512,640]{1,0:T(8,128)(2,1)} %fusion.34), channel_id=1, source_target_pairs={{0,1},{1,0},{2,3},{3,2},{4,5},{5,4},{6,7},{7,6},{8,9},{9,8},{10,11... | collective-permute-start | bytes 1966088 | tf_op jit(solution)/shard_map/ppermute | solution.py:38
  235.1 26.9 %collective-permute-start.8 = (bf16[1024,640]{1,0:T(8,128)(2,1)S(1)}, bf16[1024,640]{1,0:T(8,128)(2,1)S(1)}, u32[]{:S(2)}, u32[]{:S(2)}) collective-permute-start(bf16[1024,640]{1,0:T(8,128)(2,1)S(1)} %get-tuple-element.112), channel_id=1, source_target_pairs={{0,1},{1,0},{2,3},{3,2},{4,5},{5,4},{6,7},{7,6},{8,9},{9,8},{10,11... | collective-permute-start | bytes 3932168 | tf_op jit(solution)/shard_map/ppermute | solution.py:38
  235.8 28.6 %collective-permute-start.9 = (bf16[1024,640]{1,0:T(8,128)(2,1)S(1)}, bf16[1024,640]{1,0:T(8,128)(2,1)S(1)}, u32[]{:S(2)}, u32[]{:S(2)}) collective-permute-start(bf16[1024,640]{1,0:T(8,128)(2,1)S(1)} %get-tuple-element.112), channel_id=1, source_target_pairs={{0,2},{1,3},{2,0},{3,1},{4,6},{5,7},{6,4},{7,5},{8,10},{9,11},{10,... | collective-permute-start | bytes 3932168 | tf_op jit(solution)/shard_map/ppermute | solution.py:38
  264.0 12.5 %collective-permute-start.10 = (bf16[512,640]{1,0:T(8,128)(2,1)}, bf16[512,640]{1,0:T(8,128)(2,1)}, u32[]{:S(2)}, u32[]{:S(2)}) collective-permute-start(bf16[512,640]{1,0:T(8,128)(2,1)} %slice.290), channel_id=1, source_target_pairs={{0,2},{1,3},{2,0},{3,1},{4,6},{5,7},{6,4},{7,5},{8,10},{9,11},{10,... | collective-permute-start | bytes 1966088 | tf_op jit(solution)/shard_map/ppermute | solution.py:38
  266.4 12.3 %collective-permute-start.11 = (bf16[512,640]{1,0:T(8,128)(2,1)}, bf16[512,640]{1,0:T(8,128)(2,1)}, u32[]{:S(2)}, u32[]{:S(2)}) collective-permute-start(bf16[512,640]{1,0:T(8,128)(2,1)} %slice.291), channel_id=1, source_target_pairs={{0,1},{1,0},{2,3},{3,2},{4,5},{5,4},{6,7},{7,6},{8,9},{9,8},{10,11... | collective-permute-start | bytes 1966088 | tf_op jit(solution)/shard_map/ppermute | solution.py:38
  391.8 50.4 %copy-start.5 = (bf16[1024,896]{1,0:T(8,128)(2,1)}, bf16[1024,896]{1,0:T(8,128)(2,1)S(1)}, u32[]{:S(2)}) copy-start(bf16[1024,896]{1,0:T(8,128)(2,1)S(1)} %get-tuple-element.81.hidden_ref.refs_0_) | copy-start | bytes 5505028
  410.3 32.0 %copy-start.24 = (bf16[1024,896]{1,0:T(8,128)(2,1)S(1)}, bf16[1024,896]{1,0:T(8,128)(2,1)}, u32[]{:S(2)}) copy-start(bf16[1024,896]{1,0:T(8,128)(2,1)} %get-tuple-element.115.refs_0_.d_gate_ref) | copy-start | bytes 5505028
  410.3 32.0 %copy-start.25 = (bf16[1024,896]{1,0:T(8,128)(2,1)S(1)}, bf16[1024,896]{1,0:T(8,128)(2,1)}, u32[]{:S(2)}) copy-start(bf16[1024,896]{1,0:T(8,128)(2,1)} %get-tuple-element.119.refs_1_.d_up_ref) | copy-start | bytes 5505028
  410.3 27.8 %collective-permute-start.12 = (bf16[2,512,640]{2,1,0:T(8,128)(2,1)S(1)}, bf16[2,512,640]{2,1,0:T(8,128)(2,1)S(1)}, u32[]{:S(2)}, u32[]{:S(2)}) collective-permute-start(bf16[2,512,640]{2,1,0:T(8,128)(2,1)S(1)} %get-tuple-element.74), channel_id=1, source_target_pairs={{0,1},{1,0},{2,3},{3,2},{4,5},{5,4},{6,7},{7,6},{8,9},{9,8},{10,11... | collective-permute-start | bytes 3932168 | tf_op jit(solution)/shard_map/ppermute | solution.py:38
  412.1 27.7 %collective-permute-start.14 = (bf16[2,512,640]{2,1,0:T(8,128)(2,1)S(1)}, bf16[2,512,640]{2,1,0:T(8,128)(2,1)S(1)}, u32[]{:S(2)}, u32[]{:S(2)}) collective-permute-start(bf16[2,512,640]{2,1,0:T(8,128)(2,1)S(1)} %get-tuple-element.76), channel_id=1, source_target_pairs={{0,2},{1,3},{2,0},{3,1},{4,6},{5,7},{6,4},{7,5},{8,10},{9,11},{10,... | collective-permute-start | bytes 3932168 | tf_op jit(solution)/shard_map/ppermute | solution.py:38
  412.6 23.7 %collective-permute-start.16 = (f32[8,128]{1,0:T(8,128)S(1)}, f32[8,128]{1,0:T(8,128)S(1)}, u32[]{:S(2)}, u32[]{:S(2)}) collective-permute-start(f32[8,128]{1,0:T(8,128)S(1)} %add_bitcast_fusion), channel_id=1, source_target_pairs={{0,1},{1,0},{2,3},{3,2},{4,5},{5,4},{6,7},{7,6},{8,9},{9,8},{10,11... | collective-permute-start | bytes 12296 | tf_op jit(solution)/shard_map/ppermute | solution.py:38
  436.3 29.7 %collective-permute-start.17 = (f32[8,128]{1,0:T(8,128)S(1)}, f32[8,128]{1,0:T(8,128)S(1)}, u32[]{:S(2)}, u32[]{:S(2)}) collective-permute-start(f32[8,128]{1,0:T(8,128)S(1)} %fusion.80), channel_id=1, source_target_pairs={{0,2},{1,3},{2,0},{3,1},{4,6},{5,7},{6,4},{7,5},{8,10},{9,11},{10,... | collective-permute-start | bytes 12296 | tf_op jit(solution)/shard_map/ppermute | solution.py:38
  438.3 27.7 %collective-permute-start.13 = (bf16[512,640]{1,0:T(8,128)(2,1)S(1)}, bf16[512,640]{1,0:T(8,128)(2,1)S(1)}, u32[]{:S(2)}, u32[]{:S(2)}) collective-permute-start(bf16[512,640]{1,0:T(8,128)(2,1)S(1)} %fusion.35), channel_id=1, source_target_pairs={{0,2},{1,3},{2,0},{3,1},{4,6},{5,7},{6,4},{7,5},{8,10},{9,11},{10,... | collective-permute-start | bytes 1966088 | tf_op jit(solution)/shard_map/ppermute | solution.py:38
  441.9 24.3 %collective-permute-start.15 = (bf16[512,640]{1,0:T(8,128)(2,1)}, bf16[512,640]{1,0:T(8,128)(2,1)S(1)}, u32[]{:S(2)}, u32[]{:S(2)}) collective-permute-start(bf16[512,640]{1,0:T(8,128)(2,1)} %fusion.36), channel_id=1, source_target_pairs={{0,1},{1,0},{2,3},{3,2},{4,5},{5,4},{6,7},{7,6},{8,9},{9,8},{10,11... | collective-permute-start | bytes 1966088 | tf_op jit(solution)/shard_map/ppermute | solution.py:38
  465.9 76.8 %collective-permute-start.44 = (bf16[1280,2688]{1,0:T(8,128)(2,1)}, bf16[1280,2688]{1,0:T(8,128)(2,1)}, u32[]{:S(2)}, u32[]{:S(2)}) collective-permute-start(bf16[1280,2688]{1,0:T(8,128)(2,1)} %get-tuple-element.106), channel_id=1, source_target_pairs={{0,4},{4,0},{8,12},{12,8},{16,20},{20,16},{24,28},{28,24},{1,5},{5... | collective-permute-start | bytes 20643848 | tf_op jit(solution)/shard_map/ppermute | solution.py:719
  467.3 54.3 %slice-start = ((s8[7208960]{0:T(1024)(128)(4,1)}), s8[4194304]{0:T(1024)(128)(4,1)S(1)}, s32[]{:S(2)}) async-start(s8[7208960]{0:T(1024)(128)(4,1)} %bitcast.128), calls=%async_computation.14 | async-start | bytes 8388608
  468.1 53.4 %slice-start.1 = ((s8[7208960]{0:T(1024)(128)(4,1)}), s8[3014656]{0:T(1024)(128)(4,1)S(1)}, s32[]{:S(2)}) async-start(s8[7208960]{0:T(1024)(128)(4,1)} %bitcast.128), calls=%async_computation.15 | async-start | bytes 6029312
  472.2 30.9 %collective-permute-start.19 = (bf16[1024,640]{1,0:T(8,128)(2,1)S(1)}, bf16[1024,640]{1,0:T(8,128)(2,1)S(1)}, u32[]{:S(2)}, u32[]{:S(2)}) collective-permute-start(bf16[1024,640]{1,0:T(8,128)(2,1)S(1)} %get-tuple-element.80.own), channel_id=1, source_target_pairs={{0,1},{1,0},{2,3},{3,2},{4,5},{5,4},{6,7},{7,6},{8,9},{9,8},{10,11... | collective-permute-start | bytes 3932168 | tf_op jit(solution)/shard_map/ppermute | solution.py:38
  473.9 31.8 %collective-permute-start.20 = (bf16[1024,640]{1,0:T(8,128)(2,1)S(1)}, bf16[1024,640]{1,0:T(8,128)(2,1)S(1)}, u32[]{:S(2)}, u32[]{:S(2)}) collective-permute-start(bf16[1024,640]{1,0:T(8,128)(2,1)S(1)} %get-tuple-element.80.own), channel_id=1, source_target_pairs={{0,2},{1,3},{2,0},{3,1},{4,6},{5,7},{6,4},{7,5},{8,10},{9,11},{10,... | collective-permute-start | bytes 3932168 | tf_op jit(solution)/shard_map/ppermute | solution.py:38
  503.1 16.8 %collective-permute-start.21 = (bf16[512,640]{1,0:T(8,128)(2,1)S(1)}, bf16[512,640]{1,0:T(8,128)(2,1)S(1)}, u32[]{:S(2)}, u32[]{:S(2)}) collective-permute-start(bf16[512,640]{1,0:T(8,128)(2,1)S(1)} %slice.304), channel_id=1, source_target_pairs={{0,2},{1,3},{2,0},{3,1},{4,6},{5,7},{6,4},{7,5},{8,10},{9,11},{10,... | collective-permute-start | bytes 1966088 | tf_op jit(solution)/shard_map/ppermute | solution.py:38
  505.7 15.8 %collective-permute-start.22 = (bf16[512,640]{1,0:T(8,128)(2,1)S(1)}, bf16[512,640]{1,0:T(8,128)(2,1)S(1)}, u32[]{:S(2)}, u32[]{:S(2)}) collective-permute-start(bf16[512,640]{1,0:T(8,128)(2,1)S(1)} %slice.305), channel_id=1, source_target_pairs={{0,1},{1,0},{2,3},{3,2},{4,5},{5,4},{6,7},{7,6},{8,9},{9,8},{10,11... | collective-permute-start | bytes 1966088 | tf_op jit(solution)/shard_map/ppermute | solution.py:38
  535.9 3.7 collective-permute-start.42
  542.7 268.2 %reduce-scatter.11.cloned.1.call-start = ((), (), s32[]{:S(2)}) async-start(), calls=%async_computation.13 | async-start | bytes 8601600 | tf_op jit(solution)/shard_map/reduce_scatter | solution.py:722
  552.5 285.3 %reduce-scatter.9.cloned.1.call-start = ((), (), s32[]{:S(2)}) async-start(), calls=%async_computation.12 | async-start | bytes 9830400 | tf_op jit(solution)/shard_map/reduce_scatter | solution.py:722
  552.7 12.8 %collective-permute-start.43 = (bf16[1280,3072]{1,0:T(8,128)(2,1)}, bf16[1280,3072]{1,0:T(8,128)(2,1)}, u32[]{:S(2)}, u32[]{:S(2)}) collective-permute-start(bf16[1280,3072]{1,0:T(8,128)(2,1)} %get-tuple-element.105), channel_id=1, source_target_pairs={{0,4},{4,0},{8,12},{12,8},{16,20},{20,16},{24,28},{28,24},{1,5},{5... | collective-permute-start | bytes 23592968 | tf_op jit(solution)/shard_map/ppermute | solution.py:719
  577.8 21.4 %all-to-all-start.2 = ((bf16[4,256,640]{2,1,0:T(8,128)(2,1)}), bf16[4,256,640]{2,1,0:T(8,128)(2,1)}, u32[]{:S(2)}, u32[]{:S(2)}) async-start(bf16[4,256,640]{2,1,0:T(8,128)(2,1)} %bitcast.24), calls=%async_computation.2 | async-start | bytes 2621440 | tf_op jit(solution)/shard_map/all_to_all | solution.py:144
  618.4 7.6 collective-permute-start.23
  620.0 8.2 collective-permute-start.25
  626.7 5.2 collective-permute-start.24
  633.6 5.2 collective-permute-start.26
  643.0 36.4 %all-to-all-start.3 = ((bf16[256,4,768]{2,0,1:T(8,128)(2,1)}), bf16[256,4,768]{2,0,1:T(8,128)(2,1)}, u32[]{:S(2)}, u32[]{:S(2)}) async-start(bf16[256,4,768]{2,0,1:T(8,128)(2,1)} %bitcast.138), calls=%async_computation.3 | async-start | bytes 3145728 | tf_op jit(solution)/shard_map/all_to_all | solution.py:148
  647.3 235.2 %reduce-scatter.5.cloned.1.call-start = ((), (), s32[]{:S(2)}) async-start(), calls=%async_computation.10 | async-start | bytes 2457600 | tf_op jit(solution)/shard_map/reduce_scatter | solution.py:722
  677.4 29.5 %collective-permute-start.18 = (bf16[2,512,640]{2,1,0:T(8,128)(2,1)}, bf16[2,512,640]{2,1,0:T(8,128)(2,1)}, u32[]{:S(2)}, u32[]{:S(2)}) collective-permute-start(bf16[2,512,640]{2,1,0:T(8,128)(2,1)} %get-tuple-element.84), channel_id=1, source_target_pairs={{0,1},{1,0},{2,3},{3,2},{4,5},{5,4},{6,7},{7,6},{8,9},{9,8},{10,11... | collective-permute-start | bytes 3932168 | tf_op jit(solution)/shard_map/ppermute | solution.py:38
  703.4 66.1 %collective-permute-start.41 = (bf16[1280,768]{1,0:T(8,128)(2,1)}, bf16[1280,768]{1,0:T(8,128)(2,1)}, u32[]{:S(2)}, u32[]{:S(2)}) collective-permute-start(bf16[1280,768]{1,0:T(8,128)(2,1)} %get-tuple-element.100), channel_id=1, source_target_pairs={{0,4},{4,0},{8,12},{12,8},{16,20},{20,16},{24,28},{28,24},{1,5},{5... | collective-permute-start | bytes 5898248 | tf_op jit(solution)/shard_map/ppermute | solution.py:719
  703.4 31.5 %collective-permute-start.28 = (bf16[2,512,640]{2,1,0:T(8,128)(2,1)}, bf16[2,512,640]{2,1,0:T(8,128)(2,1)}, u32[]{:S(2)}, u32[]{:S(2)}) collective-permute-start(bf16[2,512,640]{2,1,0:T(8,128)(2,1)} %get-tuple-element.90), channel_id=1, source_target_pairs={{0,2},{1,3},{2,0},{3,1},{4,6},{5,7},{6,4},{7,5},{8,10},{9,11},{10,... | collective-permute-start | bytes 3932168 | tf_op jit(solution)/shard_map/ppermute | solution.py:38
  706.6 3.4 collective-permute-start.36
  710.1 6.9 collective-permute-start.37
  712.1 27.1 %collective-permute-start.34 = (f32[4,256]{1,0:T(4,128)S(1)}, f32[4,256]{1,0:T(4,128)S(1)}, u32[]{:S(2)}, u32[]{:S(2)}) collective-permute-start(f32[4,256]{1,0:T(4,128)S(1)} %dynamic_update_slice.45), channel_id=1, source_target_pairs={{0,1},{1,0},{2,3},{3,2},{4,5},{5,4},{6,7},{7,6},{8,9},{9,8},{10,11... | collective-permute-start | bytes 12296 | tf_op jit(solution)/shard_map/ppermute | solution.py:38
  716.9 20.6 %collective-permute-start.38 = (f32[8,320]{1,0:T(8,128)S(1)}, f32[8,320]{1,0:T(8,128)S(1)}, u32[]{:S(2)}, u32[]{:S(2)}) collective-permute-start(f32[8,320]{1,0:T(8,128)S(1)} %add.408), channel_id=1, source_target_pairs={{0,16},{4,20},{8,24},{12,28},{16,0},{20,4},{24,8},{28,12},{1,17},{... | collective-permute-start | bytes 30728 | tf_op jit(solution)/shard_map/ppermute | solution.py:138
  737.1 37.7 %collective-permute-start.30 = (bf16[2,512,640]{2,1,0:T(8,128)(2,1)}, bf16[2,512,640]{2,1,0:T(8,128)(2,1)}, u32[]{:S(2)}, u32[]{:S(2)}) collective-permute-start(bf16[2,512,640]{2,1,0:T(8,128)(2,1)} %copy-done.23), channel_id=1, source_target_pairs={{0,1},{1,0},{2,3},{3,2},{4,5},{5,4},{6,7},{7,6},{8,9},{9,8},{10,11... | collective-permute-start | bytes 3932168 | tf_op jit(solution)/shard_map/ppermute | solution.py:38
  737.6 30.4 %collective-permute-start.39 = (f32[8,320]{1,0:T(8,128)S(1)}, f32[8,320]{1,0:T(8,128)S(1)}, u32[]{:S(2)}, u32[]{:S(2)}) collective-permute-start(f32[8,320]{1,0:T(8,128)S(1)} %add.409), channel_id=1, source_target_pairs={{0,1},{1,0},{2,3},{3,2},{4,5},{5,4},{6,7},{7,6},{8,9},{9,8},{10,11... | collective-permute-start | bytes 30728 | tf_op jit(solution)/shard_map/ppermute | solution.py:38
  739.5 33.3 %collective-permute-start.35 = (f32[4,256]{1,0:T(4,128)S(1)}, f32[4,256]{1,0:T(4,128)S(1)}, u32[]{:S(2)}, u32[]{:S(2)}) collective-permute-start(f32[4,256]{1,0:T(4,128)S(1)} %add.404), channel_id=1, source_target_pairs={{0,2},{1,3},{2,0},{3,1},{4,6},{5,7},{6,4},{7,5},{8,10},{9,11},{10,... | collective-permute-start | bytes 12296 | tf_op jit(solution)/shard_map/ppermute | solution.py:38
  741.0 36.8 %collective-permute-start.32 = (bf16[2,512,640]{2,1,0:T(8,128)(2,1)}, bf16[2,512,640]{2,1,0:T(8,128)(2,1)}, u32[]{:S(2)}, u32[]{:S(2)}) collective-permute-start(bf16[2,512,640]{2,1,0:T(8,128)(2,1)} %copy-done.22), channel_id=1, source_target_pairs={{0,2},{1,3},{2,0},{3,1},{4,6},{5,7},{6,4},{7,5},{8,10},{9,11},{10,... | collective-permute-start | bytes 3932168 | tf_op jit(solution)/shard_map/ppermute | solution.py:38
  768.0 6.1 collective-permute-start.40
  772.8 18.0 %collective-permute-start.27 = (bf16[512,640]{1,0:T(8,128)(2,1)}, bf16[512,640]{1,0:T(8,128)(2,1)}, u32[]{:S(2)}, u32[]{:S(2)}) collective-permute-start(bf16[512,640]{1,0:T(8,128)(2,1)} %fusion.37), channel_id=1, source_target_pairs={{0,2},{1,3},{2,0},{3,1},{4,6},{5,7},{6,4},{7,5},{8,10},{9,11},{10,... | collective-permute-start | bytes 1966088 | tf_op jit(solution)/shard_map/ppermute | solution.py:38
  773.4 19.0 %collective-permute-start.29 = (bf16[512,640]{1,0:T(8,128)(2,1)}, bf16[512,640]{1,0:T(8,128)(2,1)S(1)}, u32[]{:S(2)}, u32[]{:S(2)}) collective-permute-start(bf16[512,640]{1,0:T(8,128)(2,1)} %fusion.38), channel_id=1, source_target_pairs={{0,1},{1,0},{2,3},{3,2},{4,5},{5,4},{6,7},{7,6},{8,9},{9,8},{10,11... | collective-permute-start | bytes 1966088 | tf_op jit(solution)/shard_map/ppermute | solution.py:38
  776.3 26.1 %collective-permute-start.31 = (bf16[512,640]{1,0:T(8,128)(2,1)S(1)}, bf16[512,640]{1,0:T(8,128)(2,1)S(1)}, u32[]{:S(2)}, u32[]{:S(2)}) collective-permute-start(bf16[512,640]{1,0:T(8,128)(2,1)S(1)} %fusion.39), channel_id=1, source_target_pairs={{0,2},{1,3},{2,0},{3,1},{4,6},{5,7},{6,4},{7,5},{8,10},{9,11},{10,... | collective-permute-start | bytes 1966088 | tf_op jit(solution)/shard_map/ppermute | solution.py:38
  779.2 24.7 %collective-permute-start.33 = (bf16[512,640]{1,0:T(8,128)(2,1)S(1)}, bf16[512,640]{1,0:T(8,128)(2,1)S(1)}, u32[]{:S(2)}, u32[]{:S(2)}) collective-permute-start(bf16[512,640]{1,0:T(8,128)(2,1)S(1)} %fusion.40), channel_id=1, source_target_pairs={{0,1},{1,0},{2,3},{3,2},{4,5},{5,4},{6,7},{7,6},{8,9},{9,8},{10,11... | collective-permute-start | bytes 1966088 | tf_op jit(solution)/shard_map/ppermute | solution.py:38
  843.3 41.3 %collective-permute-start.45 = (f32[320]{0:T(512)S(1)}, f32[320]{0:T(512)S(1)}, u32[]{:S(2)}, u32[]{:S(2)}) collective-permute-start(f32[320]{0:T(512)S(1)} %get-tuple-element.122), channel_id=1, source_target_pairs={{0,1},{1,0},{2,3},{3,2},{4,5},{5,4},{6,7},{7,6},{8,9},{9,8},{10,11... | collective-permute-start | bytes 3848 | tf_op jit(solution)/shard_map/ppermute | solution.py:38
  884.6 4.4 collective-permute-start.46
  (63 other events, 450.7 us)
Sparse Core Ops, SparseCore 0:
  88.4 140.9 all-gather.2
  231.6 124.5 all-gather.4
  542.8 33.9 reduce-scatter.6
  579.0 119.2 reduce-scatter.10
  700.4 137.2 reduce-scatter.8
  840.5 41.9 reduce-scatter.4

commit v8 on v7

--- a/solution.py
+++ b/solution.py
@@ -149,8 +149,11 @@
 
 
 def first_kernel(
-    x_ref, w_ref, rows_ref, weight_ref, own, x_sent, x_got, w_up, w_down, w_core, w_got
+    parts, x_ref, w_ref, gain_ref, *refs
 ):
+    weights, (rows_ref, weight_ref), locals_ref = refs[:3], refs[3:5], refs[5:7]
+    held, joined = refs[7:10], refs[10:12]
+    own, x_sent, x_got, w_up, w_down, w_core, w_got = refs[12:]
     me, tok = lax.axis_index("mdl"), lax.axis_index("tok")
     pairs = lax.axis_size("tok") // 2
     level, last = tok // 2, pairs - 1
@@ -206,6 +209,21 @@
     keep_w = pltpu.make_async_copy(w_ref, block(tok), own.at[1])
     keep_x.start()
     keep_w.start()
+    loads = [
+        pltpu.make_async_copy(weight, to, own.at[2 + at])
+        for at, (weight, to) in enumerate(zip(weights, held))
+    ]
+    for copy in loads:
+        copy.start()
+    for copy in loads:
+        copy.wait()
+    for (start, stop), out in zip(parts, joined):
+        count = stop - start
+        for at, source in enumerate(held):
+            value = source[:, start:stop]
+            if at < 2:
+                value = (value.astype(F32) * gain_ref[...]).astype(BF16)
+            out[:, at * count : (at + 1) * count] = value
 
     def relay(distance):
         low, high = tok - 2 * distance, tok + 2 * distance
@@ -231,6 +249,12 @@
             w_copy(block(high), high, w_core.at[high], tok ^ 1).start()
 
     relay(1)
+    stores = [
+        pltpu.make_async_copy(out, to, own.at[5 + at])
+        for at, (out, to) in enumerate(zip(joined, locals_ref))
+    ]
+    for copy in stores:
+        copy.start()
     from_x = rows_ref.at[pl.ds(0, half), cols(me ^ 1)]
     from_y = rows_ref.at[pl.ds(half, half), cols(me ^ 2)]
     top, bottom = x_copy(from_x, from_x, 2, 2), x_copy(from_y, from_y, 3, 1)
@@ -240,7 +264,7 @@
     bottom.start()
     for distance in range(2, pairs):
         relay(distance)
-    for copy in (keep_x, keep_w):
+    for copy in (keep_x, keep_w, *stores):
         copy.wait()
     for copy in (top, bottom):
         copy.wait_recv()
@@ -262,27 +286,30 @@
         w_copy(block(far), far, w_core.at[near], tok ^ 1).wait_recv()
 
 
-def first_gather(inputs, weight):
+def first_gather(inputs, weight, gain, weights, parts):
     tokens, width = inputs.shape
     shard, cols = weight.shape
     pairs = lax.axis_size("tok") // 2
     dma = pltpu.SemaphoreType.DMA
-    return pl.pallas_call(
-        first_kernel,
-        out_shape=(
-            jax.ShapeDtypeStruct((tokens, 4 * width), BF16),
-            jax.ShapeDtypeStruct((2 * pairs * shard, cols), BF16),
-        ),
-        in_specs=[pl.BlockSpec(memory_space=pltpu.VMEM)] * 2,
-        out_specs=[pl.BlockSpec(memory_space=pl.ANY)] * 2,
-        scratch_shapes=[
-            dma((2,)), dma((4,)), dma((4,)), dma((pairs,)), dma((pairs,)),
+    locals_ff = [(shard, 3 * (stop - start)) for start, stop in parts]
+    shapes = [(tokens, 4 * width), (2 * pairs * shard, cols), *locals_ff]
+    *gathered, first, second = pl.pallas_call(
+        functools.partial(first_kernel, parts),
+        out_shape=[jax.ShapeDtypeStruct(shape, BF16) for shape in shapes],
+        in_specs=[pl.BlockSpec(memory_space=pltpu.VMEM)] * 3
+        + [pl.BlockSpec(memory_space=pl.ANY)] * 3,
+        out_specs=[pl.BlockSpec(memory_space=pl.ANY)] * 4,
+        scratch_shapes=[pltpu.VMEM(array.shape, BF16) for array in weights]
+        + [pltpu.VMEM(shape, BF16) for shape in locals_ff]
+        + [
+            dma((7,)), dma((4,)), dma((4,)), dma((pairs,)), dma((pairs,)),
             dma((2 * pairs,)), dma((2 * pairs,)),
         ],
         compiler_params=pltpu.CompilerParams(
-            collective_id=0, has_side_effects=True, vmem_limit_bytes=16 << 20
+            collective_id=0, has_side_effects=True, vmem_limit_bytes=60 << 20
         ),
-    )(inputs, weight)
+    )(inputs, weight, gain, *weights)
+    return *gathered, (first, second)
 
 
 def in_order(mebibytes):
@@ -315,8 +342,10 @@
     return (distance >= 0) & (distance <= position_ref[...])
 
 
-def forward_kernel(first_ref, q_ref, kv_ref, cos_ref, sin_ref, pos_ref, out_ref, norm_ref):
-    query = turn(q_ref[...].astype(F32), cos_ref[...], sin_ref[...])
+def forward_kernel(
+    first_ref, q_ref, kv_ref, cos_ref, sin_ref, pos_ref, scale_ref, out_ref, norm_ref
+):
+    query = turn(q_ref[...].astype(F32) * scale_ref[...], cos_ref[...], sin_ref[...])
     query = (query * HEAD ** (-0.5)).astype(BF16)
     keys, values = kv_ref[:, :HEAD], kv_ref[:, HEAD:]
     scores = nt(query, keys)
@@ -329,13 +358,13 @@
 
 
 def backward_kernel(
-    first_ref, q_ref, kv_ref, cos_ref, sin_ref, pos_ref, att_ref, datt_ref, norm_ref,
+    first_ref, q_ref, kv_ref, cos_ref, sin_ref, pos_ref, scale_ref, att_ref, datt_ref, norm_ref,
     dq_ref, dkv_ref,
 ):
     head = pl.program_id(0)
     scale = HEAD ** (-0.5)
     cos, sin = cos_ref[...], sin_ref[...]
-    query = (turn(q_ref[...].astype(F32), cos, sin) * scale).astype(BF16)
+    query = (turn(q_ref[...].astype(F32) * scale_ref[...], cos, sin) * scale).astype(BF16)
     keys, values = kv_ref[:, :HEAD], kv_ref[:, HEAD:]
     scores = nt(query, keys)
     visible = seen(first_ref, pos_ref, *scores.shape)
@@ -358,7 +387,7 @@
     return pl.BlockSpec(shape, lambda head: (0,) * len(shape))
 
 
-def attention_forward(first, qkv, kv, cos, sin, pos):
+def attention_forward(first, qkv, kv, cos, sin, pos, scale):
     rows, keys = qkv.shape[0], kv.shape[0]
     head_spec = pl.BlockSpec((rows, HEAD), lambda head: (0, head))
     return pl.pallas_call(
@@ -375,15 +404,16 @@
             whole_spec((rows, HEAD // 2)),
             whole_spec((rows, HEAD // 2)),
             whole_spec((rows, 1)),
+            whole_spec((rows, 1)),
         ],
         out_specs=(head_spec, pl.BlockSpec((1, rows, 1), lambda head: (head, 0, 0))),
         compiler_params=in_order(32),
         cost_estimate=cost(4 * rows * keys * HEADS * HEAD, 4 * rows * HEADS * HEAD + 4 * keys * HEAD, rows * keys * HEADS),
-        name="attention_forward",
-    )(first, qkv, kv, cos, sin, pos)
-
-
-def attention_backward(first, qkv, kv, cos, sin, pos, att, d_att, norm):
+        name="att_f",
+    )(first, qkv, kv, cos, sin, pos, scale)
+
+
+def attention_backward(first, qkv, kv, cos, sin, pos, scale, att, d_att, norm):
     rows, keys = qkv.shape[0], kv.shape[0]
     head_spec = pl.BlockSpec((rows, HEAD), lambda head: (0, head))
     return pl.pallas_call(
@@ -400,6 +430,7 @@
             whole_spec((rows, HEAD // 2)),
             whole_spec((rows, HEAD // 2)),
             whole_spec((rows, 1)),
+            whole_spec((rows, 1)),
             head_spec,
             head_spec,
             pl.BlockSpec((1, rows, 1), lambda head: (head, 0, 0)),
@@ -407,8 +438,8 @@
         out_specs=(head_spec, whole_spec((keys, 2 * HEAD))),
         compiler_params=in_order(40),
         cost_estimate=cost(10 * rows * keys * HEADS * HEAD, 8 * rows * HEADS * HEAD + 12 * keys * HEAD, rows * keys * HEADS),
-        name="attention_backward",
-    )(first, qkv, kv, cos, sin, pos, att, d_att, norm)
+        name="att_b",
+    )(first, qkv, kv, cos, sin, pos, scale, att, d_att, norm)
 
 
 def keep_half(core_ref, total, kept, sent):
@@ -726,36 +757,41 @@
 
     qkv_cols, ff_cols = qkv_weight.shape[1], gate_weight.shape[1]
     attn_local = jnp.concatenate([scaled(qkv_weight, norm1_gain), out_weight.T], axis=1)
-    middle = -(-ff_cols // 256) * 128
+    middle = ff_cols // 256 * 128
     parts = ((0, middle), (middle, ff_cols))
-
-    def part_local(start, stop):
-        local = [scaled(w[:, start:stop], norm2_gain) for w in (gate_weight, up_weight)]
-        return jnp.concatenate([*local, down_weight[start:stop].T], axis=1)
-
-    locals_ff = [part_local(*part) for part in parts]
     if size == 4 and lax.axis_size("tok") == 8:
-        rows_in, w_attn = first_gather(inputs, after(attn_local, locals_ff[0]))
-        locals_ff = lax.optimization_barrier((*locals_ff, w_attn))[:-1]
+        rows_in, w_attn, locals_ff = first_gather(
+            inputs,
+            attn_local,
+            norm2_gain.astype(F32)[:, None],
+            (gate_weight, up_weight, down_weight.T),
+            parts,
+        )
     else:
         rows_in = gather_mdl(inputs, 1)
         w_attn = from_tok(attn_local, 0)
+        scaled_gu = [scaled(weight, norm2_gain) for weight in (gate_weight, up_weight)]
+        locals_ff = [
+            jnp.concatenate([w[:, start:stop] for w in (*scaled_gu, down_weight.T)], axis=1)
+            for start, stop in parts
+        ]
     w_qkv = w_attn[:, :qkv_cols]
     w_parts = [from_tok(local, 0) for local in locals_ff]
 
-    scale_one = row_scale(rows_in)
-    qkv_part = (nn(rows_in, w_qkv) * scale_one).astype(BF16)
-    qkv = rows_to_cols(qkv_part)
+    qkv = rows_to_cols(nn(rows_in, w_qkv).astype(BF16))
     count = qkv.shape[0]
+    scale_own = row_scale(lax.dynamic_slice_in_dim(rows_in, me * count, count, 0))
+    scale_one = row_scale(after(rows_in, qkv))
     half = HEAD // 2
     frequency = jnp.exp(jnp.arange(half, dtype=F32) * (-2.0 * math.log(10000.0) / HEAD))
     angles = positions.astype(F32)[:, None] * frequency[None, :]
     cos, sin = jnp.cos(angles), jnp.sin(angles)
-    key_rows = turn(qkv[:, head_cols : head_cols + HEAD].astype(F32), cos, sin).astype(BF16)
-    kv = gather_mdl(jnp.concatenate([key_rows, qkv[:, head_cols + HEAD :]], axis=1), 0)
+    kv_own = qkv[:, head_cols:].astype(F32) * scale_own
+    key_rows = turn(kv_own[:, :HEAD], cos, sin)
+    kv = gather_mdl(jnp.concatenate([key_rows, kv_own[:, HEAD:]], axis=1).astype(BF16), 0)
     first = (me * count).astype(jnp.int32).reshape(1)
     pos = positions[:, None]
-    attended, log_norm = attention_forward(first, qkv, kv, cos, sin, pos)
+    attended, log_norm = attention_forward(first, qkv, kv, cos, sin, pos, scale_own)
     head_block = cols_to_rows(attended)
     residual = inputs.astype(F32)
     payload, scatter = product_to_mdl((head_block,), w_attn, (qkv_cols,))
@@ -812,12 +848,12 @@
     out_grad = pair_to_tok(out_local)
     d_attended = rows_to_cols(d_head)
     d_query, d_kv = attention_backward(
-        first, qkv, kv, cos, sin, pos, attended, d_attended, log_norm
+        first, qkv, kv, cos, sin, pos, scale_own, attended, d_attended, log_norm
     )
     d_kv = scatter_mdl(d_kv.astype(BF16), 0)
     d_key = unturn(d_kv[:, :HEAD], cos, sin).astype(BF16)
     d_qkv = jnp.concatenate([d_query, d_key, d_kv[:, HEAD:].astype(BF16)], axis=1)
-    stat_one = jnp.sum(d_qkv.astype(F32) * qkv.astype(F32), axis=1)
+    stat_one = jnp.sum(d_qkv.astype(F32) * qkv.astype(F32), axis=1) * scale_own[:, 0]
     d_qkv_part = cols_to_rows(d_qkv)
     stat_rows = jnp.zeros((size, count), F32)
     stat_rows = sum_mdl(lax.dynamic_update_slice(stat_rows, stat_one[None], (me, 0)))

time: 904 us -> 896 us (level)
  local copies, waits for them, and re-layouts: 51.1 us -> 37.3 us
    unnamed x143 -> x135, local copies, waits for them, and re-layouts: 21.2 us -> 14.7 us
  transfers between devices with their start and end apart: 56 -> 56, of which waited for: 26 -> 32; matrix products, arithmetic and copies ran while one was open for 18% -> 17% of each run, Pallas kernels for 18% -> 18%
where the time goes in v8:
time: 896 us; the launch traced here: 889 us
  waiting for transfers between devices  342 us (38%)
  Pallas kernels  247 us (28%)
  other arithmetic  100 us (11%)
  matrix products  68.4 us (8%)
  starting transfers between devices  60.3 us (7%)
  local copies, waits for them, and re-layouts  37.3 us (4%)
  blocking collectives  18.6 us (2%)
  between operations  15.5 us (2%)
    ppermute x40, waiting for transfers between devices, swap(): return lax.ppermute(block, 'mdl', [(i, i ^ distance) for i in range(size)])  218 us
    pallas_call x1, Pallas kernels, first_gather(): pl.pallas_call(functools.partial(first_kernel, parts), out_shape=[jax.Sha...  70.2 us
    dot_general x7, matrix products, nn(): return jnp.dot(left_op, right_op, preferred_element_type=F32)  68.4 us
    reduce_scatter x4, waiting for transfers between devices, pair_to_tok(): lax.psum_scatter(both, 'tok', scatter_dimension=0, tiled=True, axis_index...  61.2 us
    pallas_call x4, Pallas kernels, scatter_product(): pl.pallas_call(functools.partial(payload_kernel, starts), grid_spec=pltpu...  48.9 us
    pallas_call x2, Pallas kernels, part_grad(): pl.pallas_call(part_kernel, grid=(pairs,), out_shape=(out, out), in_specs...  48.5 us
    ppermute x40, starting transfers between devices, swap(): return lax.ppermute(block, 'mdl', [(i, i ^ distance) for i in range(size)])  46.2 us
    all_to_all x2, waiting for transfers between devices, rows_to_cols(): return lax.all_to_all(block, 'mdl', split_axis=0, concat_axis=1, tiled=True)  35.1 us
  transfers between devices with their start and end apart: 56, of which 32 were waited for; matrix products, arithmetic and copies ran while one was open for 17% of the time, Pallas kernels for 18%

profile of v8, /device:TPU:0, one launch (start us, length us, event | category | flops | bytes accessed | tf_op | source)
XLA Modules:
  0.0 888.6 jit_solution(4715683867157732407)
XLA Ops:
  12.5 70.2 %shard_map.169 = (bf16[1024,2560]{1,0:T(8,128)(2,1)}, bf16[2560,1408]{1,0:T(8,128)(2,1)}, bf16[320,2688]{1,0:T(8,128)(2,1)}, bf16[320,3072]{1,0:T(8,128)(2,1)}) custom-call(bf16[1024,640]{1,0:T(8,128)(2,1)} %x_ref.1, bf16[320,1408]{1,0:T(8,128)(2,1)} %pad_maximum_fusion.3.w_ref, f32[320,1]{1,0:T(8,128)} %reshape.224.gain_ref, bf16[320,1920]{1,0:T(8,128)(2,1)} %refs_0_.1, ...), custom_call_target="tpu_custom_call" | custom-call | tf_op jit(solution)/shard_map/pallas_call | solution.py:296
  83.5 9.1 %fusion.30 = bf16[1024,768]{1,0:T(8,128)(2,1)} fusion(bf16[1024,2560]{1,0:T(8,128)(2,1)} %get-tuple-element.91.left_ref, bf16[2560,1408]{1,0:T(8,128)(2,1)} %get-tuple-element.60.refs_1_.weight_ref.refs_0_), kind=kOutput, calls=%fused_computation.61 | convolution fusion | flops 4027318272 | bytes 10747904 | tf_op jit(solution)/shard_map/dot_general | solution.py:33
  92.6 4.1 all-to-all-start
  98.5 18.1 %all-to-all-done = bf16[4,256,768]{2,1,0:T(8,128)(2,1)S(1)} async-done(((bf16[4,256,768]{2,1,0:T(8,128)(2,1)}), bf16[4,256,768]{2,1,0:T(8,128)(2,1)S(1)}, u32[]{:S(2)}, u32[]{:S(2)}) %all-to-all-start) | async-done | bytes 1572896 | tf_op jit(solution)/shard_map/all_to_all | solution.py:144
  121.5 5.5 collective-permute-done
  132.0 2.4 collective-permute-done.3
  134.5 11.2 %att_f.1 = (bf16[256,2560]{1,0:T(8,128)(2,1)S(1)}, f32[10,256,1]{2,1,0:T(8,128)S(1)}) custom-call(s32[1]{0:T(128)} %bitcast.1.first_ref, bf16[256,3072]{1,0:T(8,128)(2,1)S(1)} %bitcast.129, bf16[1024,512]{1,0:T(8,128)(2,1)S(1)} %constant_dynamic-update-slice_fusion.4.kv_ref, f32[256,128]{1,0:T(8,128)S(1)} %get-tuple-element.145.cos_ref, ...), custom_call_target="tpu_custom_call" | custom-call | flops 2684354560 | bytes 3670016 | tf_op jit(solution)/shard_map/att_f/pallas_call | solution.py:393
  145.8 18.6 %all_to_all.76 = bf16[256,4,640]{2,0,1:T(8,128)(2,1)} all-to-all(bf16[256,4,640]{2,0,1:T(8,128)(2,1)S(1)} %bitcast.138), channel_id=1, replica_groups=mesh['tok'=8,'mdl'=4] {'mdl'}, dimensions={1} | all-to-all | bytes 2621440 | tf_op jit(solution)/shard_map/all_to_all | solution.py:148
  164.5 7.8 shard_map.170
  173.9 25.5 %collective-permute-done.4 = bf16[2,512,640]{2,1,0:T(8,128)(2,1)S(1)} collective-permute-done((bf16[2,512,640]{2,1,0:T(8,128)(2,1)S(1)}, bf16[2,512,640]{2,1,0:T(8,128)(2,1)S(1)}, u32[]{:S(2)}, u32[]{:S(2)}) %collective-permute-start.4) | collective-permute-done | bytes 1310752 | tf_op jit(solution)/shard_map/ppermute | solution.py:38
  204.5 10.0 %collective-permute-done.5 = bf16[512,640]{1,0:T(8,128)(2,1)S(1)} collective-permute-done((bf16[512,640]{1,0:T(8,128)(2,1)}, bf16[512,640]{1,0:T(8,128)(2,1)S(1)}, u32[]{:S(2)}, u32[]{:S(2)}) %collective-permute-start.5) | collective-permute-done | bytes 655392 | tf_op jit(solution)/shard_map/ppermute | solution.py:38
  218.3 2.7 broadcast_in_dim.31
  225.4 24.3 %collective-permute-done.8 = bf16[1024,640]{1,0:T(8,128)(2,1)S(1)} collective-permute-done((bf16[1024,640]{1,0:T(8,128)(2,1)S(1)}, bf16[1024,640]{1,0:T(8,128)(2,1)S(1)}, u32[]{:S(2)}, u32[]{:S(2)}) %collective-permute-start.8) | collective-permute-done | bytes 1310752 | tf_op jit(solution)/shard_map/ppermute | solution.py:38
  253.3 2.7 collective-permute-start.11
  259.1 4.7 collective-permute-done.10
  267.2 3.7 fusion
  270.9 5.7 fusion.1.rows_ref
  276.6 9.3 %fusion.12 = f32[896,1024]{0,1:T(8,128)S(1)} fusion(bf16[1024,2560]{1,0:T(8,128)(2,1)} %above_ref.2, bf16[2560,2688]{1,0:T(8,128)(2,1)} %all-gather.3.cloned.1.call-done.refs_2_.refs_1_), kind=kOutput, calls=%fused_computation.17 | convolution fusion | flops 4697620480 | bytes 13500416 | tf_op jit(solution)/shard_map/dot_general | solution.py:33
  285.9 8.0 fusion.8
  293.9 9.4 %add_reduce_fusion.1 = (f32[1024]{0:T(1024)S(1)}, bf16[1024,896]{1,0:T(8,128)(2,1)S(1)}, bf16[1024,896]{1,0:T(8,128)(2,1)S(1)}, bf16[1024,896]{1,0:T(8,128)(2,1)S(1)}) fusion(f32[1024,896]{1,0:T(8,128)S(1)} %fusion.8, f32[896,1024]{0,1:T(8,128)S(1)} %fusion.12, bf16[1024,2560]{1,0:T(8,128)(2,1)S(1)} %copy-done.42, ...), kind=kOutput, calls=%fused_computation.32 | convolution fusion | flops 4723309568 | bytes 22679552 | tf_op jit(solution)/shard_map/dot_general | solution.py:33
  303.3 23.5 %shard_map.171 = (bf16[1280,2688]{1,0:T(8,128)(2,1)}, bf16[1280,2688]{1,0:T(8,128)(2,1)}) custom-call(s32[1]{0:T(128)} %bitcast.14.core_ref, bf16[1024,2560]{1,0:T(8,128)(2,1)} %fusion.1.rows_ref, bf16[1024,2560]{1,0:T(8,128)(2,1)} %above_ref.2, bf16[1024,896]{1,0:T(8,128)(2,1)S(1)} %get-tuple-element.71.d_gate_ref.refs_0_, ...), custom_call_target="tpu_custom_call" | custom-call | flops 14092861440 | bytes 29753344 | tf_op jit(solution)/shard_map/pallas_call | solution.py:533
  326.8 15.4 %shard_map.172.refs_3_ = f32[1024,2560]{1,0:T(8,128)} custom-call(bf16[1024,896]{1,0:T(8,128)(2,1)S(1)} %get-tuple-element.71.d_gate_ref.refs_0_, bf16[1024,896]{1,0:T(8,128)(2,1)S(1)} %get-tuple-element.119.d_up_ref.refs_1_, bf16[2560,2688]{1,0:T(8,128)(2,1)} %all-gather.3.cloned.1.call-done.refs_2_.refs_1_), custom_call_target="tpu_custom_call" | custom-call | flops 9395240960 | bytes 24248320 | tf_op jit(solution)/shard_map/pallas_call | solution.py:605
  342.2 8.0 all-gather.5.cloned.1.call-done.refs_2_.refs_1_
  350.2 10.7 %fusion.2 = f32[1024,1024]{1,0:T(8,128)} fusion(bf16[1024,2560]{1,0:T(8,128)(2,1)} %above_ref.2, bf16[2560,3072]{1,0:T(8,128)(2,1)} %all-gather.5.cloned.1.call-done.refs_2_.refs_1_), kind=kOutput, calls=%fused_computation.7 | convolution fusion | flops 5368709120 | bytes 14680064 | tf_op jit(solution)/shard_map/dot_general | solution.py:33
  360.9 8.9 %fusion.4 = f32[1024,1024]{1,0:T(8,128)} fusion(bf16[1024,2560]{1,0:T(8,128)(2,1)} %fusion.1.rows_ref, bf16[2560,3072]{1,0:T(8,128)(2,1)S(1)} %copy-done.38), kind=kOutput, calls=%fused_computation.9 | convolution fusion | flops 5368709120 | bytes 14680064 | tf_op jit(solution)/shard_map/dot_general | solution.py:33
  369.9 13.0 %fusion.67 = (bf16[1024,1024]{1,0:T(8,128)(2,1)}, f32[1024]{0:T(1024)S(1)}, bf16[1024,1024]{1,0:T(8,128)(2,1)}, bf16[1024,1024]{1,0:T(8,128)(2,1)}) fusion(f32[1024,1024]{1,0:T(8,128)} %fusion.2, f32[1024,1024]{1,0:T(8,128)} %fusion.4, bf16[1024,2560]{1,0:T(8,128)(2,1)S(1)} %bitcast.137, bf16[2560,3072]{1,0:T(8,128)(2,1)S(1)} %copy-done.38), kind=kOutput, calls=%fused_computation.162 | convolution fusion | flops 5398068224 | bytes 25169920 | tf_op jit(solution)/shard_map/dot_general | solution.py:33
  382.8 18.7 %shard_map.173 = (bf16[2,512,640]{2,1,0:T(8,128)(2,1)S(1)}, bf16[2,512,640]{2,1,0:T(8,128)(2,1)S(1)}, bf16[2,512,640]{2,1,0:T(8,128)(2,1)S(1)}, bf16[2,512,640]{2,1,0:T(8,128)(2,1)S(1)}) custom-call(s32[1]{0:T(128)} %bitcast.me_ref, bf16[1024,1024]{1,0:T(8,128)(2,1)} %get-tuple-element.113.refs_0_.d_gate_ref, ...), custom_call_target="tpu_custom_call" | custom-call | flops 10737418240 | bytes 25165824 | tf_op jit(solution)/shard_map/pallas_call | solution.py:646
  405.2 28.7 %collective-permute-done.16 = f32[8,128]{1,0:T(8,128)S(1)} collective-permute-done((f32[8,128]{1,0:T(8,128)S(1)}, f32[8,128]{1,0:T(8,128)S(1)}, u32[]{:S(2)}, u32[]{:S(2)}) %collective-permute-start.16) | collective-permute-done | bytes 4128 | tf_op jit(solution)/shard_map/ppermute | solution.py:38
  438.6 25.0 %shard_map.174 = (bf16[1280,3072]{1,0:T(8,128)(2,1)}, bf16[1280,3072]{1,0:T(8,128)(2,1)}) custom-call(s32[1]{0:T(128)} %bitcast.14.core_ref, bf16[1024,2560]{1,0:T(8,128)(2,1)} %fusion.1.rows_ref, bf16[1024,2560]{1,0:T(8,128)(2,1)} %above_ref.2, bf16[1024,1024]{1,0:T(8,128)(2,1)S(1)} %copy-done.27, bf16[1024,1024]{1,0:T(8,128)(2,1)S(1)} %copy-done.28, ...), custom_call_target="tpu_custom_call" | custom-call | flops 16106127360 | bytes 32505856 | tf_op jit(solution)/shard_map/pallas_call | solution.py:533
  466.1 3.9 fusion.70
  471.1 27.8 %collective-permute-done.20.along_y = bf16[1024,640]{1,0:T(8,128)(2,1)S(1)} collective-permute-done((bf16[1024,640]{1,0:T(8,128)(2,1)S(1)}, bf16[1024,640]{1,0:T(8,128)(2,1)S(1)}, u32[]{:S(2)}, u32[]{:S(2)}) %collective-permute-start.20) | collective-permute-done | bytes 1310752 | tf_op jit(solution)/shard_map/ppermute | solution.py:38
  501.9 11.4 %collective-permute-done.22.bottom = bf16[512,640]{1,0:T(8,128)(2,1)S(1)} collective-permute-done((bf16[512,640]{1,0:T(8,128)(2,1)S(1)}, bf16[512,640]{1,0:T(8,128)(2,1)S(1)}, u32[]{:S(2)}, u32[]{:S(2)}) %collective-permute-start.22) | collective-permute-done | bytes 655392 | tf_op jit(solution)/shard_map/ppermute | solution.py:38
  513.5 6.4 shard_map.177
  519.9 7.8 shard_map.180
  527.7 3.7 collective-permute-done.42
  531.4 3.0 add_convert_fusion.3
  534.5 9.7 %add_convert_fusion.1 = bf16[1280,2688]{1,0:T(8,128)(2,1)} fusion(bf16[1280,2688]{1,0:T(8,128)(2,1)} %collective-permute-done.43, bf16[1280,2688]{1,0:T(8,128)(2,1)} %get-tuple-element.67), kind=kLoop, calls=%fused_computation.1 | loop fusion | flops 13762560 | bytes 20643840 | tf_op jit(solution)/shard_map/convert_element_type | solution.py:751
  544.5 12.6 %collective-permute-done.44 = bf16[1280,3072]{1,0:T(8,128)(2,1)} collective-permute-done((bf16[1280,3072]{1,0:T(8,128)(2,1)}, bf16[1280,3072]{1,0:T(8,128)(2,1)}, u32[]{:S(2)}, u32[]{:S(2)}) %collective-permute-start.44) | collective-permute-done | bytes 7864352 | tf_op jit(solution)/shard_map/ppermute | solution.py:750
  557.1 12.3 %add_convert_fusion = bf16[1280,3072]{1,0:T(8,128)(2,1)} fusion(bf16[1280,3072]{1,0:T(8,128)(2,1)} %collective-permute-done.44, bf16[1280,3072]{1,0:T(8,128)(2,1)} %get-tuple-element.78), kind=kLoop, calls=%fused_computation | loop fusion | flops 15728640 | bytes 23592960 | tf_op jit(solution)/shard_map/convert_element_type | solution.py:751
  569.4 4.7 all-to-all-start.2
  574.1 17.0 %all-to-all-done.2 = bf16[4,256,640]{2,1,0:T(8,128)(2,1)} async-done(((bf16[4,256,640]{2,1,0:T(8,128)(2,1)}), bf16[4,256,640]{2,1,0:T(8,128)(2,1)}, u32[]{:S(2)}, u32[]{:S(2)}) %all-to-all-start.2) | async-done | bytes 1310752 | tf_op jit(solution)/shard_map/all_to_all | solution.py:144
  595.4 15.6 %att_b.1 = (bf16[256,2560]{1,0:T(8,128)(2,1)S(1)}, f32[1024,512]{1,0:T(8,128)S(1)}) custom-call(s32[1]{0:T(128)} %bitcast.1.first_ref, bf16[256,3072]{1,0:T(8,128)(2,1)S(1)} %bitcast.130, bf16[1024,512]{1,0:T(8,128)(2,1)S(1)} %copy-done.14, f32[256,128]{1,0:T(8,128)S(1)} %copy-done.22, f32[256,128]{1,0:T(8,128)S(1)} %copy-done.20, s32[256,1]{1,0:T(8,128)S(1)} %copy-done.16, ...), custom_call_target="tpu_custom_call" | custom-call | flops 6710886400 | bytes 8388608 | tf_op jit(solution)/shard_map/att_b/pallas_call | solution.py:419
  614.1 4.7 collective-permute-done.23
  621.1 3.7 collective-permute-done.24
  628.0 3.8 collective-permute-done.26
  636.1 4.4 all-to-all-start.3
  640.5 3.7 multiply_reduce_fusion
  644.2 13.6 %shard_map.175.refs_2_ = f32[1024,2560]{1,0:T(8,128)} custom-call(bf16[1024,896]{1,0:T(8,128)(2,1)S(1)} %get-tuple-element.81.hidden_ref.refs_0_, bf16[2560,2688]{1,0:T(8,128)(2,1)} %all-gather.3.cloned.1.call-done.refs_2_.refs_1_), custom_call_target="tpu_custom_call" | custom-call | flops 4697620480 | bytes 24248320 | tf_op jit(solution)/shard_map/pallas_call | solution.py:605
  657.7 14.1 %shard_map.176 = (bf16[2,512,640]{2,1,0:T(8,128)(2,1)}, bf16[2,512,640]{2,1,0:T(8,128)(2,1)}, bf16[2,512,640]{2,1,0:T(8,128)(2,1)S(1)}, bf16[2,512,640]{2,1,0:T(8,128)(2,1)S(1)}) custom-call(s32[1]{0:T(128)} %bitcast.me_ref, bf16[1024,1024]{1,0:T(8,128)(2,1)} %get-tuple-element.80.hidden_ref.refs_0_, ...), custom_call_target="tpu_custom_call" | custom-call | flops 5368709120 | bytes 23068672 | tf_op jit(solution)/shard_map/pallas_call | solution.py:646
  675.9 8.2 shard_map.178
  689.6 9.1 %shard_map.179 = (bf16[1280,768]{1,0:T(8,128)(2,1)S(1)}, bf16[1280,768]{1,0:T(8,128)(2,1)}, f32[2560,1]{1,0:T(8,128)S(1)}) custom-call(s32[1]{0:T(128)} %bitcast.14.core_ref, bf16[1024,2560]{1,0:T(8,128)(2,1)} %get-tuple-element.91.left_ref, bf16[1024,768]{1,0:T(8,128)(2,1)S(1)} %multiply_convert_fusion.2.right_ref, ...), custom_call_target="tpu_custom_call" | custom-call | flops 4026531840 | bytes 10747904 | tf_op jit(solution)/shard_map/pallas_call | solution.py:500
  704.9 2.5 multiply_reduce_fusion.1
  709.3 2.3 collective-permute-done.37
  712.1 18.2 %collective-permute-done.28 = bf16[2,512,640]{2,1,0:T(8,128)(2,1)} collective-permute-done((bf16[2,512,640]{2,1,0:T(8,128)(2,1)}, bf16[2,512,640]{2,1,0:T(8,128)(2,1)}, u32[]{:S(2)}, u32[]{:S(2)}) %collective-permute-start.28) | collective-permute-done | bytes 1310752 | tf_op jit(solution)/shard_map/ppermute | solution.py:38
  738.1 3.3 add_convert_fusion.2
  741.4 21.7 %collective-permute-done.35 = f32[4,256]{1,0:T(4,128)S(1)} collective-permute-done((f32[4,256]{1,0:T(4,128)S(1)}, f32[4,256]{1,0:T(4,128)S(1)}, u32[]{:S(2)}, u32[]{:S(2)}) %collective-permute-start.35) | collective-permute-done | bytes 4128 | tf_op jit(solution)/shard_map/ppermute | solution.py:38
  770.7 10.3 %collective-permute-done.27 = bf16[512,640]{1,0:T(8,128)(2,1)} collective-permute-done((bf16[512,640]{1,0:T(8,128)(2,1)}, bf16[512,640]{1,0:T(8,128)(2,1)}, u32[]{:S(2)}, u32[]{:S(2)}) %collective-permute-start.27) | collective-permute-done | bytes 655392 | tf_op jit(solution)/shard_map/ppermute | solution.py:38
  784.0 9.8 %collective-permute-done.33 = bf16[512,640]{1,0:T(8,128)(2,1)S(1)} collective-permute-done((bf16[512,640]{1,0:T(8,128)(2,1)S(1)}, bf16[512,640]{1,0:T(8,128)(2,1)S(1)}, u32[]{:S(2)}, u32[]{:S(2)}) %collective-permute-start.33) | collective-permute-done | bytes 655392 | tf_op jit(solution)/shard_map/ppermute | solution.py:38
  797.4 3.4 fusion.22
  802.8 3.2 fusion.74
  806.0 23.3 %reduce-scatter.11.cloned.1.call-done = bf16[320,3072]{1,0:T(8,128)(2,1)} async-done(((bf16[1280,3072]{1,0:T(8,128)(2,1)}), bf16[320,3072]{1,0:T(8,128)(2,1)}) %reduce-scatter.11.cloned.1.call-update) | async-done | bytes 1966096 | tf_op jit(solution)/shard_map/reduce_scatter | solution.py:753
  831.9 2.9 fusion.26
  836.3 38.0 %reduce-scatter.5.cloned.1.call-done = bf16[320,768]{1,0:T(8,128)(2,1)} async-done(((bf16[1280,768]{1,0:T(8,128)(2,1)}), bf16[320,768]{1,0:T(8,128)(2,1)}) %reduce-scatter.5.cloned.1.call-update) | async-done | bytes 491536 | tf_op jit(solution)/shard_map/reduce_scatter | solution.py:753
  877.9 2.9 maximum_bitcast_fusion
  (315 shorter events, 125.0 us)
Async XLA Ops:
  7.2 269.4 %all-gather.3.cloned.1.call-start = ((), (), s32[]{:S(2)}) async-start(), calls=%async_computation.8 | async-start | bytes 15482880 | tf_op jit(solution)/shard_map/all_gather | solution.py:745
  82.8 267.4 %all-gather.5.cloned.1.call-start = ((), (), s32[]{:S(2)}) async-start(), calls=%async_computation.9 | async-start | bytes 17694720 | tf_op jit(solution)/shard_map/all_gather | solution.py:745
  92.6 23.9 %all-to-all-start = ((bf16[4,256,768]{2,1,0:T(8,128)(2,1)}), bf16[4,256,768]{2,1,0:T(8,128)(2,1)S(1)}, u32[]{:S(2)}, u32[]{:S(2)}) async-start(bf16[4,256,768]{2,1,0:T(8,128)(2,1)} %bitcast.4), calls=%async_computation | async-start | bytes 3145728 | tf_op jit(solution)/shard_map/all_to_all | solution.py:144
  96.7 704.1 %reduce-scatter.7.cloned.1.call-start = ((), (), s32[]{:S(2)}) async-start(), calls=%async_computation.11 | async-start | bytes 2048000 | tf_op jit(solution)/shard_map/reduce_scatter | solution.py:753
  118.3 27.3 %copy-start.19 = (f32[256,128]{1,0:T(8,128)}, f32[256,128]{1,0:T(8,128)S(1)}, u32[]{:S(2)}) copy-start(f32[256,128]{1,0:T(8,128)S(1)} %get-tuple-element.144.sin_ref) | copy-start | bytes 393220
  118.3 27.3 %copy-start.21 = (f32[256,128]{1,0:T(8,128)}, f32[256,128]{1,0:T(8,128)S(1)}, u32[]{:S(2)}) copy-start(f32[256,128]{1,0:T(8,128)S(1)} %get-tuple-element.145.cos_ref) | copy-start | bytes 393220
  119.2 7.8 collective-permute-start
  120.6 7.9 collective-permute-start.1
  127.0 5.0 collective-permute-start.2
  129.4 5.0 collective-permute-start.3
  172.3 27.1 %copy-start.12 = (bf16[2,512,640]{2,1,0:T(8,128)(2,1)}, bf16[2,512,640]{2,1,0:T(8,128)(2,1)S(1)}, u32[]{:S(2)}) copy-start(bf16[2,512,640]{2,1,0:T(8,128)(2,1)S(1)} %get-tuple-element.62) | copy-start | bytes 3932164
  172.3 27.1 %collective-permute-start.4 = (bf16[2,512,640]{2,1,0:T(8,128)(2,1)S(1)}, bf16[2,512,640]{2,1,0:T(8,128)(2,1)S(1)}, u32[]{:S(2)}, u32[]{:S(2)}) collective-permute-start(bf16[2,512,640]{2,1,0:T(8,128)(2,1)S(1)} %get-tuple-element.63), channel_id=1, source_target_pairs={{0,1},{1,0},{2,3},{3,2},{4,5},{5,4},{6,7},{7,6},{8,9},{9,8},{10,11... | collective-permute-start | bytes 3932168 | tf_op jit(solution)/shard_map/ppermute | solution.py:38
  173.3 28.6 %collective-permute-start.6 = (bf16[2,512,640]{2,1,0:T(8,128)(2,1)S(1)}, bf16[2,512,640]{2,1,0:T(8,128)(2,1)S(1)}, u32[]{:S(2)}, u32[]{:S(2)}) collective-permute-start(bf16[2,512,640]{2,1,0:T(8,128)(2,1)S(1)} %get-tuple-element.65), channel_id=1, source_target_pairs={{0,2},{1,3},{2,0},{3,1},{4,6},{5,7},{6,4},{7,5},{8,10},{9,11},{10,... | collective-permute-start | bytes 3932168 | tf_op jit(solution)/shard_map/ppermute | solution.py:38
  200.6 13.9 %collective-permute-start.5 = (bf16[512,640]{1,0:T(8,128)(2,1)}, bf16[512,640]{1,0:T(8,128)(2,1)S(1)}, u32[]{:S(2)}, u32[]{:S(2)}) collective-permute-start(bf16[512,640]{1,0:T(8,128)(2,1)} %fusion.34), channel_id=1, source_target_pairs={{0,2},{1,3},{2,0},{3,1},{4,6},{5,7},{6,4},{7,5},{8,10},{9,11},{10,... | collective-permute-start | bytes 1966088 | tf_op jit(solution)/shard_map/ppermute | solution.py:38
  204.0 12.7 %collective-permute-start.7 = (bf16[512,640]{1,0:T(8,128)(2,1)}, bf16[512,640]{1,0:T(8,128)(2,1)}, u32[]{:S(2)}, u32[]{:S(2)}) collective-permute-start(bf16[512,640]{1,0:T(8,128)(2,1)} %fusion.35), channel_id=1, source_target_pairs={{0,1},{1,0},{2,3},{3,2},{4,5},{5,4},{6,7},{7,6},{8,9},{9,8},{10,11... | collective-permute-start | bytes 1966088 | tf_op jit(solution)/shard_map/ppermute | solution.py:38
  222.7 27.0 %collective-permute-start.8 = (bf16[1024,640]{1,0:T(8,128)(2,1)S(1)}, bf16[1024,640]{1,0:T(8,128)(2,1)S(1)}, u32[]{:S(2)}, u32[]{:S(2)}) collective-permute-start(bf16[1024,640]{1,0:T(8,128)(2,1)S(1)} %get-tuple-element.112), channel_id=1, source_target_pairs={{0,1},{1,0},{2,3},{3,2},{4,5},{5,4},{6,7},{7,6},{8,9},{9,8},{10,11... | collective-permute-start | bytes 3932168 | tf_op jit(solution)/shard_map/ppermute | solution.py:38
  223.9 27.4 %collective-permute-start.9 = (bf16[1024,640]{1,0:T(8,128)(2,1)S(1)}, bf16[1024,640]{1,0:T(8,128)(2,1)S(1)}, u32[]{:S(2)}, u32[]{:S(2)}) collective-permute-start(bf16[1024,640]{1,0:T(8,128)(2,1)S(1)} %get-tuple-element.112), channel_id=1, source_target_pairs={{0,2},{1,3},{2,0},{3,1},{4,6},{5,7},{6,4},{7,5},{8,10},{9,11},{10,... | collective-permute-start | bytes 3932168 | tf_op jit(solution)/shard_map/ppermute | solution.py:38
  250.6 13.3 %collective-permute-start.10 = (bf16[512,640]{1,0:T(8,128)(2,1)}, bf16[512,640]{1,0:T(8,128)(2,1)S(1)}, u32[]{:S(2)}, u32[]{:S(2)}) collective-permute-start(bf16[512,640]{1,0:T(8,128)(2,1)} %slice.270), channel_id=1, source_target_pairs={{0,2},{1,3},{2,0},{3,1},{4,6},{5,7},{6,4},{7,5},{8,10},{9,11},{10,... | collective-permute-start | bytes 1966088 | tf_op jit(solution)/shard_map/ppermute | solution.py:38
  253.3 11.8 %collective-permute-start.11 = (bf16[512,640]{1,0:T(8,128)(2,1)}, bf16[512,640]{1,0:T(8,128)(2,1)}, u32[]{:S(2)}, u32[]{:S(2)}) collective-permute-start(bf16[512,640]{1,0:T(8,128)(2,1)} %slice.271), channel_id=1, source_target_pairs={{0,1},{1,0},{2,3},{3,2},{4,5},{5,4},{6,7},{7,6},{8,9},{9,8},{10,11... | collective-permute-start | bytes 1966088 | tf_op jit(solution)/shard_map/ppermute | solution.py:38
  382.8 55.8 %copy-start.28 = (bf16[1024,1024]{1,0:T(8,128)(2,1)S(1)}, bf16[1024,1024]{1,0:T(8,128)(2,1)}, u32[]{:S(2)}) copy-start(bf16[1024,1024]{1,0:T(8,128)(2,1)} %get-tuple-element.117.refs_1_.d_up_ref) | copy-start | bytes 6291460
  401.6 37.0 %copy-start.27 = (bf16[1024,1024]{1,0:T(8,128)(2,1)S(1)}, bf16[1024,1024]{1,0:T(8,128)(2,1)}, u32[]{:S(2)}) copy-start(bf16[1024,1024]{1,0:T(8,128)(2,1)} %get-tuple-element.113.refs_0_.d_gate_ref) | copy-start | bytes 6291460
  401.6 32.8 %collective-permute-start.14 = (bf16[2,512,640]{2,1,0:T(8,128)(2,1)S(1)}, bf16[2,512,640]{2,1,0:T(8,128)(2,1)S(1)}, u32[]{:S(2)}, u32[]{:S(2)}) collective-permute-start(bf16[2,512,640]{2,1,0:T(8,128)(2,1)S(1)} %get-tuple-element.75), channel_id=1, source_target_pairs={{0,2},{1,3},{2,0},{3,1},{4,6},{5,7},{6,4},{7,5},{8,10},{9,11},{10,... | collective-permute-start | bytes 3932168 | tf_op jit(solution)/shard_map/ppermute | solution.py:38
  403.1 33.0 %collective-permute-start.12 = (bf16[2,512,640]{2,1,0:T(8,128)(2,1)S(1)}, bf16[2,512,640]{2,1,0:T(8,128)(2,1)S(1)}, u32[]{:S(2)}, u32[]{:S(2)}) collective-permute-start(bf16[2,512,640]{2,1,0:T(8,128)(2,1)S(1)} %get-tuple-element.73), channel_id=1, source_target_pairs={{0,1},{1,0},{2,3},{3,2},{4,5},{5,4},{6,7},{7,6},{8,9},{9,8},{10,11... | collective-permute-start | bytes 3932168 | tf_op jit(solution)/shard_map/ppermute | solution.py:38
  404.6 29.3 %collective-permute-start.16 = (f32[8,128]{1,0:T(8,128)S(1)}, f32[8,128]{1,0:T(8,128)S(1)}, u32[]{:S(2)}, u32[]{:S(2)}) collective-permute-start(f32[8,128]{1,0:T(8,128)S(1)} %add_bitcast_fusion), channel_id=1, source_target_pairs={{0,1},{1,0},{2,3},{3,2},{4,5},{5,4},{6,7},{7,6},{8,9},{9,8},{10,11... | collective-permute-start | bytes 12296 | tf_op jit(solution)/shard_map/ppermute | solution.py:38
  405.2 129.4 %collective-permute-start.43 = (bf16[1280,2688]{1,0:T(8,128)(2,1)}, bf16[1280,2688]{1,0:T(8,128)(2,1)}, u32[]{:S(2)}, u32[]{:S(2)}) collective-permute-start(bf16[1280,2688]{1,0:T(8,128)(2,1)} %get-tuple-element.105), channel_id=1, source_target_pairs={{0,4},{4,0},{8,12},{12,8},{16,20},{20,16},{24,28},{28,24},{1,5},{5... | collective-permute-start | bytes 20643848 | tf_op jit(solution)/shard_map/ppermute | solution.py:750
  433.9 29.8 %collective-permute-start.17 = (f32[8,128]{1,0:T(8,128)S(1)}, f32[8,128]{1,0:T(8,128)S(1)}, u32[]{:S(2)}, u32[]{:S(2)}) collective-permute-start(f32[8,128]{1,0:T(8,128)S(1)} %fusion.82), channel_id=1, source_target_pairs={{0,2},{1,3},{2,0},{3,1},{4,6},{5,7},{6,4},{7,5},{8,10},{9,11},{10,... | collective-permute-start | bytes 12296 | tf_op jit(solution)/shard_map/ppermute | solution.py:38
  434.6 29.1 %collective-permute-start.15 = (bf16[512,640]{1,0:T(8,128)(2,1)S(1)}, bf16[512,640]{1,0:T(8,128)(2,1)S(1)}, u32[]{:S(2)}, u32[]{:S(2)}) collective-permute-start(bf16[512,640]{1,0:T(8,128)(2,1)S(1)} %fusion.37), channel_id=1, source_target_pairs={{0,1},{1,0},{2,3},{3,2},{4,5},{5,4},{6,7},{7,6},{8,9},{9,8},{10,11... | collective-permute-start | bytes 1966088 | tf_op jit(solution)/shard_map/ppermute | solution.py:38
  437.1 26.9 %collective-permute-start.13 = (bf16[512,640]{1,0:T(8,128)(2,1)}, bf16[512,640]{1,0:T(8,128)(2,1)}, u32[]{:S(2)}, u32[]{:S(2)}) collective-permute-start(bf16[512,640]{1,0:T(8,128)(2,1)} %fusion.36), channel_id=1, source_target_pairs={{0,2},{1,3},{2,0},{3,1},{4,6},{5,7},{6,4},{7,5},{8,10},{9,11},{10,... | collective-permute-start | bytes 1966088 | tf_op jit(solution)/shard_map/ppermute | solution.py:38
  464.0 49.5 %slice-start = ((s8[7208960]{0:T(1024)(128)(4,1)}), s8[4194304]{0:T(1024)(128)(4,1)S(1)}, s32[]{:S(2)}) async-start(s8[7208960]{0:T(1024)(128)(4,1)} %bitcast.126), calls=%async_computation.14 | async-start | bytes 8388608
  466.1 47.4 %slice-start.1 = ((s8[7208960]{0:T(1024)(128)(4,1)}), s8[3014656]{0:T(1024)(128)(4,1)S(1)}, s32[]{:S(2)}) async-start(s8[7208960]{0:T(1024)(128)(4,1)} %bitcast.126), calls=%async_computation.15 | async-start | bytes 6029312
  470.0 28.9 %collective-permute-start.20 = (bf16[1024,640]{1,0:T(8,128)(2,1)S(1)}, bf16[1024,640]{1,0:T(8,128)(2,1)S(1)}, u32[]{:S(2)}, u32[]{:S(2)}) collective-permute-start(bf16[1024,640]{1,0:T(8,128)(2,1)S(1)} %get-tuple-element.79.own), channel_id=1, source_target_pairs={{0,2},{1,3},{2,0},{3,1},{4,6},{5,7},{6,4},{7,5},{8,10},{9,11},{10,... | collective-permute-start | bytes 3932168 | tf_op jit(solution)/shard_map/ppermute | solution.py:38
  470.5 29.1 %collective-permute-start.19 = (bf16[1024,640]{1,0:T(8,128)(2,1)S(1)}, bf16[1024,640]{1,0:T(8,128)(2,1)S(1)}, u32[]{:S(2)}, u32[]{:S(2)}) collective-permute-start(bf16[1024,640]{1,0:T(8,128)(2,1)S(1)} %get-tuple-element.79.own), channel_id=1, source_target_pairs={{0,1},{1,0},{2,3},{3,2},{4,5},{5,4},{6,7},{7,6},{8,9},{9,8},{10,11... | collective-permute-start | bytes 3932168 | tf_op jit(solution)/shard_map/ppermute | solution.py:38
  499.0 14.3 %collective-permute-start.22 = (bf16[512,640]{1,0:T(8,128)(2,1)S(1)}, bf16[512,640]{1,0:T(8,128)(2,1)S(1)}, u32[]{:S(2)}, u32[]{:S(2)}) collective-permute-start(bf16[512,640]{1,0:T(8,128)(2,1)S(1)} %slice.285), channel_id=1, source_target_pairs={{0,1},{1,0},{2,3},{3,2},{4,5},{5,4},{6,7},{7,6},{8,9},{9,8},{10,11... | collective-permute-start | bytes 1966088 | tf_op jit(solution)/shard_map/ppermute | solution.py:38
  499.7 13.8 %collective-permute-start.21 = (bf16[512,640]{1,0:T(8,128)(2,1)S(1)}, bf16[512,640]{1,0:T(8,128)(2,1)S(1)}, u32[]{:S(2)}, u32[]{:S(2)}) collective-permute-start(bf16[512,640]{1,0:T(8,128)(2,1)S(1)} %slice.284), channel_id=1, source_target_pairs={{0,2},{1,3},{2,0},{3,1},{4,6},{5,7},{6,4},{7,5},{8,10},{9,11},{10,... | collective-permute-start | bytes 1966088 | tf_op jit(solution)/shard_map/ppermute | solution.py:38
  527.7 3.7 collective-permute-start.42
  534.5 268.3 %reduce-scatter.9.cloned.1.call-start = ((), (), s32[]{:S(2)}) async-start(), calls=%async_computation.12 | async-start | bytes 8601600 | tf_op jit(solution)/shard_map/reduce_scatter | solution.py:753
  544.3 285.1 %reduce-scatter.11.cloned.1.call-start = ((), (), s32[]{:S(2)}) async-start(), calls=%async_computation.13 | async-start | bytes 9830400 | tf_op jit(solution)/shard_map/reduce_scatter | solution.py:753
  544.3 12.8 %collective-permute-start.44 = (bf16[1280,3072]{1,0:T(8,128)(2,1)}, bf16[1280,3072]{1,0:T(8,128)(2,1)}, u32[]{:S(2)}, u32[]{:S(2)}) collective-permute-start(bf16[1280,3072]{1,0:T(8,128)(2,1)} %get-tuple-element.106), channel_id=1, source_target_pairs={{0,4},{4,0},{8,12},{12,8},{16,20},{20,16},{24,28},{28,24},{1,5},{5... | collective-permute-start | bytes 23592968 | tf_op jit(solution)/shard_map/ppermute | solution.py:750
  569.4 21.7 %all-to-all-start.2 = ((bf16[4,256,640]{2,1,0:T(8,128)(2,1)}), bf16[4,256,640]{2,1,0:T(8,128)(2,1)}, u32[]{:S(2)}, u32[]{:S(2)}) async-start(bf16[4,256,640]{2,1,0:T(8,128)(2,1)} %bitcast.24), calls=%async_computation.2 | async-start | bytes 2621440 | tf_op jit(solution)/shard_map/all_to_all | solution.py:144
  611.3 7.5 collective-permute-start.23
  613.6 7.5 collective-permute-start.25
  619.6 5.2 collective-permute-start.24
  626.6 5.2 collective-permute-start.26
  636.1 39.9 %all-to-all-start.3 = ((bf16[256,4,768]{2,0,1:T(8,128)(2,1)}), bf16[256,4,768]{2,0,1:T(8,128)(2,1)}, u32[]{:S(2)}, u32[]{:S(2)}) async-start(bf16[256,4,768]{2,0,1:T(8,128)(2,1)} %bitcast.124), calls=%async_computation.3 | async-start | bytes 3145728 | tf_op jit(solution)/shard_map/all_to_all | solution.py:148
  640.4 233.8 %reduce-scatter.5.cloned.1.call-start = ((), (), s32[]{:S(2)}) async-start(), calls=%async_computation.10 | async-start | bytes 2457600 | tf_op jit(solution)/shard_map/reduce_scatter | solution.py:753
  674.0 28.1 %collective-permute-start.18 = (bf16[2,512,640]{2,1,0:T(8,128)(2,1)}, bf16[2,512,640]{2,1,0:T(8,128)(2,1)}, u32[]{:S(2)}, u32[]{:S(2)}) collective-permute-start(bf16[2,512,640]{2,1,0:T(8,128)(2,1)} %get-tuple-element.83), channel_id=1, source_target_pairs={{0,1},{1,0},{2,3},{3,2},{4,5},{5,4},{6,7},{7,6},{8,9},{9,8},{10,11... | collective-permute-start | bytes 3932168 | tf_op jit(solution)/shard_map/ppermute | solution.py:38
  698.8 39.3 %collective-permute-start.41 = (bf16[1280,768]{1,0:T(8,128)(2,1)}, bf16[1280,768]{1,0:T(8,128)(2,1)}, u32[]{:S(2)}, u32[]{:S(2)}) collective-permute-start(bf16[1280,768]{1,0:T(8,128)(2,1)} %get-tuple-element.100), channel_id=1, source_target_pairs={{0,4},{4,0},{8,12},{12,8},{16,20},{20,16},{24,28},{28,24},{1,5},{5... | collective-permute-start | bytes 5898248 | tf_op jit(solution)/shard_map/ppermute | solution.py:750
  698.8 31.5 %collective-permute-start.28 = (bf16[2,512,640]{2,1,0:T(8,128)(2,1)}, bf16[2,512,640]{2,1,0:T(8,128)(2,1)}, u32[]{:S(2)}, u32[]{:S(2)}) collective-permute-start(bf16[2,512,640]{2,1,0:T(8,128)(2,1)} %get-tuple-element.89), channel_id=1, source_target_pairs={{0,2},{1,3},{2,0},{3,1},{4,6},{5,7},{6,4},{7,5},{8,10},{9,11},{10,... | collective-permute-start | bytes 3932168 | tf_op jit(solution)/shard_map/ppermute | solution.py:38
  704.9 2.5 collective-permute-start.36
  707.4 4.1 collective-permute-start.37
  707.6 26.9 %collective-permute-start.34 = (f32[4,256]{1,0:T(4,128)S(1)}, f32[4,256]{1,0:T(4,128)S(1)}, u32[]{:S(2)}, u32[]{:S(2)}) collective-permute-start(f32[4,256]{1,0:T(4,128)S(1)} %dynamic_update_slice.45), channel_id=1, source_target_pairs={{0,1},{1,0},{2,3},{3,2},{4,5},{5,4},{6,7},{7,6},{8,9},{9,8},{10,11... | collective-permute-start | bytes 12296 | tf_op jit(solution)/shard_map/ppermute | solution.py:38
  711.6 22.2 %collective-permute-start.38 = (f32[8,320]{1,0:T(8,128)S(1)}, f32[8,320]{1,0:T(8,128)S(1)}, u32[]{:S(2)}, u32[]{:S(2)}) collective-permute-start(f32[8,320]{1,0:T(8,128)S(1)} %add.436), channel_id=1, source_target_pairs={{0,16},{4,20},{8,24},{12,28},{16,0},{20,4},{24,8},{28,12},{1,17},{... | collective-permute-start | bytes 30728 | tf_op jit(solution)/shard_map/ppermute | solution.py:138
  732.3 33.7 %collective-permute-start.32 = (bf16[2,512,640]{2,1,0:T(8,128)(2,1)}, bf16[2,512,640]{2,1,0:T(8,128)(2,1)}, u32[]{:S(2)}, u32[]{:S(2)}) collective-permute-start(bf16[2,512,640]{2,1,0:T(8,128)(2,1)} %copy-done.24), channel_id=1, source_target_pairs={{0,2},{1,3},{2,0},{3,1},{4,6},{5,7},{6,4},{7,5},{8,10},{9,11},{10,... | collective-permute-start | bytes 3932168 | tf_op jit(solution)/shard_map/ppermute | solution.py:38
  733.8 3.8 collective-permute-start.39
  734.6 28.5 %collective-permute-start.35 = (f32[4,256]{1,0:T(4,128)S(1)}, f32[4,256]{1,0:T(4,128)S(1)}, u32[]{:S(2)}, u32[]{:S(2)}) collective-permute-start(f32[4,256]{1,0:T(4,128)S(1)} %add.432), channel_id=1, source_target_pairs={{0,2},{1,3},{2,0},{3,1},{4,6},{5,7},{6,4},{7,5},{8,10},{9,11},{10,... | collective-permute-start | bytes 12296 | tf_op jit(solution)/shard_map/ppermute | solution.py:38
  734.9 34.0 %collective-permute-start.30 = (bf16[2,512,640]{2,1,0:T(8,128)(2,1)}, bf16[2,512,640]{2,1,0:T(8,128)(2,1)}, u32[]{:S(2)}, u32[]{:S(2)}) collective-permute-start(bf16[2,512,640]{2,1,0:T(8,128)(2,1)} %copy-done.23), channel_id=1, source_target_pairs={{0,1},{1,0},{2,3},{3,2},{4,5},{5,4},{6,7},{7,6},{8,9},{9,8},{10,11... | collective-permute-start | bytes 3932168 | tf_op jit(solution)/shard_map/ppermute | solution.py:38
  737.6 27.6 %collective-permute-start.40 = (f32[8,320]{1,0:T(8,128)S(1)}, f32[8,320]{1,0:T(8,128)S(1)}, u32[]{:S(2)}, u32[]{:S(2)}) collective-permute-start(f32[8,320]{1,0:T(8,128)S(1)} %add.438), channel_id=1, source_target_pairs={{0,2},{1,3},{2,0},{3,1},{4,6},{5,7},{6,4},{7,5},{8,10},{9,11},{10,... | collective-permute-start | bytes 30728 | tf_op jit(solution)/shard_map/ppermute | solution.py:38
  741.4 27.5 %copy-start.7 = (bf16[2,512,640]{2,1,0:T(8,128)(2,1)S(1)}, bf16[2,512,640]{2,1,0:T(8,128)(2,1)}, u32[]{:S(2)}) copy-start(bf16[2,512,640]{2,1,0:T(8,128)(2,1)} %copy-done.6) | copy-start | bytes 3932164
  763.1 17.9 %collective-permute-start.27 = (bf16[512,640]{1,0:T(8,128)(2,1)}, bf16[512,640]{1,0:T(8,128)(2,1)}, u32[]{:S(2)}, u32[]{:S(2)}) collective-permute-start(bf16[512,640]{1,0:T(8,128)(2,1)} %fusion.38), channel_id=1, source_target_pairs={{0,2},{1,3},{2,0},{3,1},{4,6},{5,7},{6,4},{7,5},{8,10},{9,11},{10,... | collective-permute-start | bytes 1966088 | tf_op jit(solution)/shard_map/ppermute | solution.py:38
  764.6 18.1 %collective-permute-start.29 = (bf16[512,640]{1,0:T(8,128)(2,1)}, bf16[512,640]{1,0:T(8,128)(2,1)S(1)}, u32[]{:S(2)}, u32[]{:S(2)}) collective-permute-start(bf16[512,640]{1,0:T(8,128)(2,1)} %fusion.39), channel_id=1, source_target_pairs={{0,1},{1,0},{2,3},{3,2},{4,5},{5,4},{6,7},{7,6},{8,9},{9,8},{10,11... | collective-permute-start | bytes 1966088 | tf_op jit(solution)/shard_map/ppermute | solution.py:38
  767.5 26.4 %collective-permute-start.33 = (bf16[512,640]{1,0:T(8,128)(2,1)S(1)}, bf16[512,640]{1,0:T(8,128)(2,1)S(1)}, u32[]{:S(2)}, u32[]{:S(2)}) collective-permute-start(bf16[512,640]{1,0:T(8,128)(2,1)S(1)} %fusion.41), channel_id=1, source_target_pairs={{0,1},{1,0},{2,3},{3,2},{4,5},{5,4},{6,7},{7,6},{8,9},{9,8},{10,11... | collective-permute-start | bytes 1966088 | tf_op jit(solution)/shard_map/ppermute | solution.py:38
  770.1 25.2 %collective-permute-start.31 = (bf16[512,640]{1,0:T(8,128)(2,1)S(1)}, bf16[512,640]{1,0:T(8,128)(2,1)S(1)}, u32[]{:S(2)}, u32[]{:S(2)}) collective-permute-start(bf16[512,640]{1,0:T(8,128)(2,1)S(1)} %fusion.40), channel_id=1, source_target_pairs={{0,2},{1,3},{2,0},{3,1},{4,6},{5,7},{6,4},{7,5},{8,10},{9,11},{10,... | collective-permute-start | bytes 1966088 | tf_op jit(solution)/shard_map/ppermute | solution.py:38
  834.8 41.5 %collective-permute-start.45 = (f32[320]{0:T(512)S(1)}, f32[320]{0:T(512)S(1)}, u32[]{:S(2)}, u32[]{:S(2)}) collective-permute-start(f32[320]{0:T(512)S(1)} %get-tuple-element.122), channel_id=1, source_target_pairs={{0,1},{1,0},{2,3},{3,2},{4,5},{5,4},{6,7},{7,6},{8,9},{9,8},{10,11... | collective-permute-start | bytes 3848 | tf_op jit(solution)/shard_map/ppermute | solution.py:38
  876.4 4.3 collective-permute-start.46
  (59 other events, 494.2 us)
Sparse Core Ops, SparseCore 0:
  82.9 124.8 all-gather.2
  209.5 140.6 all-gather.4
  534.6 33.7 reduce-scatter.6
  570.5 119.2 reduce-scatter.8
  691.9 137.3 reduce-scatter.10
  832.1 42.1 reduce-scatter.4

commit v9 on v8

--- a/solution.py
+++ b/solution.py
@@ -436,7 +436,7 @@
             pl.BlockSpec((1, rows, 1), lambda head: (head, 0, 0)),
         ],
         out_specs=(head_spec, whole_spec((keys, 2 * HEAD))),
-        compiler_params=in_order(40),
+        compiler_params=in_order(60),
         cost_estimate=cost(10 * rows * keys * HEADS * HEAD, 8 * rows * HEADS * HEAD + 12 * keys * HEAD, rows * keys * HEADS),
         name="att_b",
     )(first, qkv, kv, cos, sin, pos, scale, att, d_att, norm)
@@ -544,6 +544,31 @@
     )(core_index(), rows, above, d_gate, d_up, hidden)
 
 
+def join_kernel(kept_ref, got_ref, right_ref, out_ref):
+    cols = kept_ref.shape[1]
+    out_ref[:, :cols] = (kept_ref[...].astype(F32) + got_ref[...].astype(F32)).astype(BF16)
+    out_ref[:, cols:] = right_ref[...]
+
+
+def join(kept, got, right):
+    rows, cols = kept.shape
+    width = cols + right.shape[1]
+    if cols % 128:
+        both = (kept.astype(F32) + got.astype(F32)).astype(BF16)
+        return jnp.concatenate([both, right], axis=1)
+    step = rows // 4
+    left_spec = pl.BlockSpec((step, cols), lambda at: (at, 0))
+    return pl.pallas_call(
+        join_kernel,
+        grid=(4,),
+        out_shape=jax.ShapeDtypeStruct((rows, width), BF16),
+        in_specs=[left_spec, left_spec, pl.BlockSpec((step, right.shape[1]), lambda at: (at, 0))],
+        out_specs=pl.BlockSpec((step, width), lambda at: (at, 0)),
+        compiler_params=in_order(32),
+        cost_estimate=cost(rows * cols, 2 * rows * (2 * width + cols)),
+    )(kept, got, right)
+
+
 def pieces_grad_kernel(me_ref, core_ref, own, along_x, along_y, top, bottom, right_ref, kept, sent):
     at = pl.program_id(0)
     half = top.shape[0]
@@ -744,11 +769,16 @@
     def from_tok(weight, dim):
         return lax.all_gather(weight, "tok", axis=dim, tiled=True)
 
-    def pair_to_tok(local):
-        kept, sent = local
+    def from_pair(sent):
         count = lax.axis_size("tok")
-        got = lax.ppermute(sent, "tok", [(i, i ^ 1) for i in range(count)])
-        both = (kept.astype(F32) + got.astype(F32)).astype(BF16)
+        return lax.ppermute(sent, "tok", [(i, i ^ 1) for i in range(count)])
+
+    def pair_sum(local):
+        kept, got = local[0], from_pair(local[1])
+        return (kept.astype(F32) + got.astype(F32)).astype(BF16)
+
+    def to_tok(both):
+        count = lax.axis_size("tok")
         groups = [list(range(core, count, 2)) for core in range(2)]
         total = lax.psum_scatter(
             both, "tok", scatter_dimension=0, tiled=True, axis_index_groups=groups
@@ -781,7 +811,6 @@
     qkv = rows_to_cols(nn(rows_in, w_qkv).astype(BF16))
     count = qkv.shape[0]
     scale_own = row_scale(lax.dynamic_slice_in_dim(rows_in, me * count, count, 0))
-    scale_one = row_scale(after(rows_in, qkv))
     half = HEAD // 2
     frequency = jnp.exp(jnp.arange(half, dtype=F32) * (-2.0 * math.log(10000.0) / HEAD))
     angles = positions.astype(F32)[:, None] * frequency[None, :]
@@ -823,7 +852,7 @@
             d_gate = after(d_gate, local[0])
             partial = (sum_products((d_gate, d_up), weight, starts),)
             rows, above, _ = lax.optimization_barrier((rows, above, local[0]))
-        sums.append(pair_to_tok(local))
+        sums.append(to_tok(pair_sum(local)))
     d_two = scatter(payload)
     stat_two = sum_mdl(stat_two.reshape(8, -1)).reshape(-1, 1) * (1.0 / features)
     scale_mixed = scale_two * mixed
@@ -838,15 +867,18 @@
     )
     if size == 4 and lax.axis_size("tok") == 8:
         pieces = gather_pieces(d_mixed_b)
+        scale_one = row_scale(after(rows_in, pieces[1]))
         d_head = pieces_product(pieces, w_attn, qkv_cols, head_block.shape[1])
         heads_later = after(head_block, d_head)
         out_local = pieces_grad(pieces, heads_later)
     else:
+        scale_one = row_scale(rows_in)
         d_mixed_rows = gather_mdl(d_mixed_b, 1)
         d_head = nn(d_mixed_rows, w_attn[:, qkv_cols:]).astype(BF16)
         out_local = pair_grad(d_mixed_rows, head_block)
-    out_grad = pair_to_tok(out_local)
+    out_both = pair_sum(out_local)
     d_attended = rows_to_cols(d_head)
+    *ffn_payload, _ = lax.optimization_barrier((*ffn_payload, d_attended))
     d_query, d_kv = attention_backward(
         first, qkv, kv, cos, sin, pos, scale_own, attended, d_attended, log_norm
     )
@@ -858,10 +890,13 @@
     stat_rows = jnp.zeros((size, count), F32)
     stat_rows = sum_mdl(lax.dynamic_update_slice(stat_rows, stat_one[None], (me, 0)))
     stat_one = stat_rows.reshape(-1, 1) * (1.0 / features)
-    payload, scatter = product_to_mdl((d_qkv_part,), w_attn, (0,))
-    d_scaled = (after(d_qkv_part, payload[0]).astype(F32) * scale_one).astype(BF16)
-    *qkv_local, gain_one = pair_grad(rows_in, d_scaled, w_attn)
-    qkv_sum = pair_to_tok(qkv_local)
+    d_scaled = (d_qkv_part.astype(F32) * scale_one).astype(BF16)
+    kept, sent, gain_one = pair_grad(rows_in, d_scaled, w_attn)
+    got = from_pair(sent)
+    both = join(kept, got, out_both)
+    attn_sum = to_tok(both)
+    qkv_sum, out_grad = attn_sum[:, :qkv_cols], attn_sum[:, qkv_cols:].T
+    payload, scatter = product_to_mdl((after(d_qkv_part, kept),), w_attn, (0,))
     d_one = scatter(payload)
     ffn_sum = ffn_scatter(ffn_payload, d_qkv_part)
     block_out = (mixed + ffn_sum).astype(BF16)
@@ -884,7 +919,6 @@
         gate_late.astype(F32) * gate_sum + up_late.astype(F32) * up_sum, axis=1
     )
     gate_grad, up_grad = unfold(gate_sum, norm2_late), unfold(up_sum, norm2_late)
-    out_grad = out_grad.T
     gain_two_grad = sum_mdl(gain_two)
     gain_one = sum_mdl(sum_tok(gain_one.reshape(8, -1))).reshape(-1)
     shard = norm1_gain.shape[0]

time: 896 us -> 979 us (1.093)
  waiting for transfers between devices: 342 us -> 432 us
  other arithmetic: 100 us -> 87.1 us
    reduce_scatter x4 -> x3, waiting for transfers between devices: 61.2 us -> 140 us  [to_tok(): lax.psum_scatter(both, 'tok', scatter_dimension=0, tiled=True, axis_index...]
  transfers between devices with their start and end apart: 56 -> 55, of which waited for: 32 -> 36; matrix products, arithmetic and copies ran while one was open for 17% -> 13% of each run, Pallas kernels for 18% -> 14%
where the time goes in v9:
time: 979 us; the launch traced here: 971 us
  waiting for transfers between devices  432 us (44%)
  Pallas kernels  253 us (26%)
  other arithmetic  87.1 us (9%)
  matrix products  68.3 us (7%)
  starting transfers between devices  56.8 us (6%)
  local copies, waits for them, and re-layouts  40.5 us (4%)
  blocking collectives  18.6 us (2%)
  between operations  15.2 us (2%)
    ppermute x40, waiting for transfers between devices, swap(): return lax.ppermute(block, 'mdl', [(i, i ^ distance) for i in range(size)])  222 us
    reduce_scatter x3, waiting for transfers between devices, to_tok(): lax.psum_scatter(both, 'tok', scatter_dimension=0, tiled=True, axis_index...  140 us
    pallas_call x1, Pallas kernels, first_gather(): pl.pallas_call(functools.partial(first_kernel, parts), out_shape=[jax.Sha...  70.2 us
    dot_general x7, matrix products, nn(): return jnp.dot(left_op, right_op, preferred_element_type=F32)  68.3 us
    pallas_call x4, Pallas kernels, scatter_product(): pl.pallas_call(functools.partial(payload_kernel, starts), grid_spec=pltpu...  50.8 us
    pallas_call x2, Pallas kernels, part_grad(): pl.pallas_call(part_kernel, grid=(pairs,), out_shape=(out, out), in_specs...  49.2 us
    ppermute x40, starting transfers between devices, swap(): return lax.ppermute(block, 'mdl', [(i, i ^ distance) for i in range(size)])  42.7 us
    all_to_all x2, waiting for transfers between devices, rows_to_cols(): return lax.all_to_all(block, 'mdl', split_axis=0, concat_axis=1, tiled=True)  32.1 us
  transfers between devices with their start and end apart: 55, of which 36 were waited for; matrix products, arithmetic and copies ran while one was open for 13% of the time, Pallas kernels for 14%

profile of v9, /device:TPU:0, one launch (start us, length us, event | category | flops | bytes accessed | tf_op | source)
XLA Modules:
  0.0 971.4 jit_solution(15515356491471821994)
XLA Ops:
  12.5 70.2 %shard_map.169 = (bf16[1024,2560]{1,0:T(8,128)(2,1)}, bf16[2560,1408]{1,0:T(8,128)(2,1)}, bf16[320,2688]{1,0:T(8,128)(2,1)}, bf16[320,3072]{1,0:T(8,128)(2,1)}) custom-call(bf16[1024,640]{1,0:T(8,128)(2,1)} %x_ref.1, bf16[320,1408]{1,0:T(8,128)(2,1)} %pad_maximum_fusion.3.w_ref, f32[320,1]{1,0:T(8,128)} %reshape.224.gain_ref, bf16[320,1920]{1,0:T(8,128)(2,1)} %refs_0_.1, ...), custom_call_target="tpu_custom_call" | custom-call | tf_op jit(solution)/shard_map/pallas_call | solution.py:296
  83.5 9.1 fusion.30
  92.6 4.1 all-to-all-start
  98.4 18.1 %all-to-all-done = bf16[4,256,768]{2,1,0:T(8,128)(2,1)S(1)} async-done(((bf16[4,256,768]{2,1,0:T(8,128)(2,1)}), bf16[4,256,768]{2,1,0:T(8,128)(2,1)S(1)}, u32[]{:S(2)}, u32[]{:S(2)}) %all-to-all-start) | async-done | bytes 1572896 | tf_op jit(solution)/shard_map/all_to_all | solution.py:144
  121.5 5.5 collective-permute-done
  132.0 2.4 collective-permute-done.3
  134.4 11.2 %att_f.1 = (bf16[256,2560]{1,0:T(8,128)(2,1)S(1)}, f32[10,256,1]{2,1,0:T(8,128)S(1)}) custom-call(s32[1]{0:T(128)} %bitcast.1.first_ref, bf16[256,3072]{1,0:T(8,128)(2,1)S(1)} %bitcast.130, bf16[1024,512]{1,0:T(8,128)(2,1)S(1)} %constant_dynamic-update-slice_fusion.4.kv_ref, f32[256,128]{1,0:T(8,128)S(1)} %get-tuple-element.153.cos_ref, ...), custom_call_target="tpu_custom_call" | custom-call | flops 2684354560 | bytes 3670016 | tf_op jit(solution)/shard_map/att_f/pallas_call | solution.py:393
  145.8 18.6 %all_to_all.76 = bf16[256,4,640]{2,0,1:T(8,128)(2,1)} all-to-all(bf16[256,4,640]{2,0,1:T(8,128)(2,1)S(1)} %bitcast.139), channel_id=1, replica_groups=mesh['tok'=8,'mdl'=4] {'mdl'}, dimensions={1} | all-to-all | bytes 2621440 | tf_op jit(solution)/shard_map/all_to_all | solution.py:148
  164.4 7.8 shard_map.170
  173.9 25.5 %collective-permute-done.4 = bf16[2,512,640]{2,1,0:T(8,128)(2,1)S(1)} collective-permute-done((bf16[2,512,640]{2,1,0:T(8,128)(2,1)S(1)}, bf16[2,512,640]{2,1,0:T(8,128)(2,1)S(1)}, u32[]{:S(2)}, u32[]{:S(2)}) %collective-permute-start.4) | collective-permute-done | bytes 1310752 | tf_op jit(solution)/shard_map/ppermute | solution.py:38
  204.4 10.1 %collective-permute-done.5 = bf16[512,640]{1,0:T(8,128)(2,1)S(1)} collective-permute-done((bf16[512,640]{1,0:T(8,128)(2,1)}, bf16[512,640]{1,0:T(8,128)(2,1)S(1)}, u32[]{:S(2)}, u32[]{:S(2)}) %collective-permute-start.5) | collective-permute-done | bytes 655392 | tf_op jit(solution)/shard_map/ppermute | solution.py:38
  218.0 2.9 broadcast_in_dim.31
  225.0 24.1 %collective-permute-done.8 = bf16[1024,640]{1,0:T(8,128)(2,1)S(1)} collective-permute-done((bf16[1024,640]{1,0:T(8,128)(2,1)S(1)}, bf16[1024,640]{1,0:T(8,128)(2,1)S(1)}, u32[]{:S(2)}, u32[]{:S(2)}) %collective-permute-start.8) | collective-permute-done | bytes 1310752 | tf_op jit(solution)/shard_map/ppermute | solution.py:38
  253.1 2.3 collective-permute-start.11
  258.6 4.7 collective-permute-done.10
  266.4 3.6 fusion
  270.0 5.7 fusion.1.rows_ref
  275.8 9.2 fusion.12
  285.0 8.0 fusion.8
  293.0 9.4 add_reduce_fusion.1
  302.4 24.2 %shard_map.171 = (bf16[1280,2688]{1,0:T(8,128)(2,1)}, bf16[1280,2688]{1,0:T(8,128)(2,1)}) custom-call(s32[1]{0:T(128)} %bitcast.14.core_ref, bf16[1024,2560]{1,0:T(8,128)(2,1)} %fusion.1.rows_ref, bf16[1024,2560]{1,0:T(8,128)(2,1)} %above_ref.2, bf16[1024,896]{1,0:T(8,128)(2,1)S(1)} %get-tuple-element.75.d_gate_ref.refs_0_, ...), custom_call_target="tpu_custom_call" | custom-call | flops 14092861440 | bytes 29753344 | tf_op jit(solution)/shard_map/pallas_call | solution.py:533
  326.6 15.4 %shard_map.172.refs_3_ = f32[1024,2560]{1,0:T(8,128)} custom-call(bf16[1024,896]{1,0:T(8,128)(2,1)S(1)} %get-tuple-element.75.d_gate_ref.refs_0_, bf16[1024,896]{1,0:T(8,128)(2,1)S(1)} %get-tuple-element.127.d_up_ref.refs_1_, bf16[2560,2688]{1,0:T(8,128)(2,1)} %all-gather.3.cloned.1.call-done.refs_2_.refs_1_), custom_call_target="tpu_custom_call" | custom-call | flops 9395240960 | bytes 24248320 | tf_op jit(solution)/shard_map/pallas_call | solution.py:630
  342.0 8.2 all-gather.5.cloned.1.call-done.refs_2_.refs_1_
  350.2 10.7 %fusion.2 = f32[1024,1024]{1,0:T(8,128)} fusion(bf16[1024,2560]{1,0:T(8,128)(2,1)} %above_ref.2, bf16[2560,3072]{1,0:T(8,128)(2,1)} %all-gather.5.cloned.1.call-done.refs_2_.refs_1_), kind=kOutput, calls=%fused_computation.7 | convolution fusion | flops 5368709120 | bytes 14680064 | tf_op jit(solution)/shard_map/dot_general | solution.py:33
  360.9 8.9 fusion.4
  369.9 13.0 %fusion.67 = (bf16[1024,1024]{1,0:T(8,128)(2,1)}, f32[1024]{0:T(1024)S(1)}, bf16[1024,1024]{1,0:T(8,128)(2,1)}, bf16[1024,1024]{1,0:T(8,128)(2,1)}) fusion(f32[1024,1024]{1,0:T(8,128)} %fusion.2, f32[1024,1024]{1,0:T(8,128)} %fusion.4, bf16[1024,2560]{1,0:T(8,128)(2,1)S(1)} %bitcast.138, bf16[2560,3072]{1,0:T(8,128)(2,1)S(1)} %copy-done.32), kind=kOutput, calls=%fused_computation.161 | convolution fusion | flops 5398068224 | bytes 25169920 | tf_op jit(solution)/shard_map/dot_general | solution.py:33
  382.8 18.7 %shard_map.173 = (bf16[2,512,640]{2,1,0:T(8,128)(2,1)S(1)}, bf16[2,512,640]{2,1,0:T(8,128)(2,1)S(1)}, bf16[2,512,640]{2,1,0:T(8,128)(2,1)S(1)}, bf16[2,512,640]{2,1,0:T(8,128)(2,1)S(1)}) custom-call(s32[1]{0:T(128)} %bitcast.me_ref, bf16[1024,1024]{1,0:T(8,128)(2,1)} %get-tuple-element.121.refs_0_.d_gate_ref, ...), custom_call_target="tpu_custom_call" | custom-call | flops 10737418240 | bytes 25165824 | tf_op jit(solution)/shard_map/pallas_call | solution.py:671
  405.2 28.7 %collective-permute-done.16 = f32[8,128]{1,0:T(8,128)S(1)} collective-permute-done((f32[8,128]{1,0:T(8,128)S(1)}, f32[8,128]{1,0:T(8,128)S(1)}, u32[]{:S(2)}, u32[]{:S(2)}) %collective-permute-start.16) | collective-permute-done | bytes 4128 | tf_op jit(solution)/shard_map/ppermute | solution.py:38
  437.8 25.0 %shard_map.174 = (bf16[1280,3072]{1,0:T(8,128)(2,1)}, bf16[1280,3072]{1,0:T(8,128)(2,1)}) custom-call(s32[1]{0:T(128)} %bitcast.14.core_ref, bf16[1024,2560]{1,0:T(8,128)(2,1)} %fusion.1.rows_ref, bf16[1024,2560]{1,0:T(8,128)(2,1)} %above_ref.2, bf16[1024,1024]{1,0:T(8,128)(2,1)S(1)} %copy-done.22, bf16[1024,1024]{1,0:T(8,128)(2,1)S(1)} %copy-done.23, ...), custom_call_target="tpu_custom_call" | custom-call | flops 16106127360 | bytes 32505856 | tf_op jit(solution)/shard_map/pallas_call | solution.py:533
  464.8 4.0 fusion.70
  469.9 27.8 %collective-permute-done.19.along_y = bf16[1024,640]{1,0:T(8,128)(2,1)S(1)} collective-permute-done((bf16[1024,640]{1,0:T(8,128)(2,1)S(1)}, bf16[1024,640]{1,0:T(8,128)(2,1)S(1)}, u32[]{:S(2)}, u32[]{:S(2)}) %collective-permute-start.19) | collective-permute-done | bytes 1310752 | tf_op jit(solution)/shard_map/ppermute | solution.py:38
  498.5 2.2 collective-permute-start.20
  500.7 11.4 %collective-permute-done.21.bottom = bf16[512,640]{1,0:T(8,128)(2,1)S(1)} collective-permute-done((bf16[512,640]{1,0:T(8,128)(2,1)S(1)}, bf16[512,640]{1,0:T(8,128)(2,1)S(1)}, u32[]{:S(2)}, u32[]{:S(2)}) %collective-permute-start.21) | collective-permute-done | bytes 655392 | tf_op jit(solution)/shard_map/ppermute | solution.py:38
  512.3 6.4 shard_map.177
  518.8 4.5 all-to-all-start.2
  523.3 14.0 %all-to-all-done.2 = bf16[4,256,640]{2,1,0:T(8,128)(2,1)} async-done(((bf16[4,256,640]{2,1,0:T(8,128)(2,1)}), bf16[4,256,640]{2,1,0:T(8,128)(2,1)}, u32[]{:S(2)}, u32[]{:S(2)}) %all-to-all-start.2) | async-done | bytes 1310752 | tf_op jit(solution)/shard_map/all_to_all | solution.py:144
  537.3 2.5 copy.120
  539.8 18.4 %att_b.1 = (bf16[256,2560]{1,0:T(8,128)(2,1)}, f32[1024,512]{1,0:T(8,128)}) custom-call(s32[1]{0:T(128)} %bitcast.1.first_ref, bf16[256,3072]{1,0:T(8,128)(2,1)} %bitcast.131, bf16[1024,512]{1,0:T(8,128)(2,1)} %copy-done.13, f32[256,128]{1,0:T(8,128)} %copy-done.19, f32[256,128]{1,0:T(8,128)} %copy-done.18, s32[256,1]{1,0:T(8,128)} %copy-done.16, ...), custom_call_target="tpu_custom_call" | custom-call | flops 6710886400 | bytes 8388608 | tf_op jit(solution)/shard_map/att_b/pallas_call | solution.py:419
  562.3 5.8 collective-permute-done.23
  569.9 4.3 collective-permute-done.24
  576.3 5.0 collective-permute-done.26
  585.7 4.3 all-to-all-start.3
  590.2 3.7 multiply_reduce_fusion
  593.9 7.7 shard_map.180
  601.9 4.5 all-to-all-done.3
  608.1 9.2 shard_map.178
  617.8 3.7 collective-permute-done.41.got_ref
  624.3 10.1 %add_convert_fusion.1 = bf16[1280,2688]{1,0:T(8,128)(2,1)} fusion(bf16[1280,2688]{1,0:T(8,128)(2,1)} %collective-permute-done.43, bf16[1280,2688]{1,0:T(8,128)(2,1)} %get-tuple-element.71), kind=kLoop, calls=%fused_computation.1 | loop fusion | flops 13762560 | bytes 20643840 | tf_op jit(solution)/shard_map/convert_element_type | solution.py:778
  634.7 12.6 %collective-permute-done.44 = bf16[1280,3072]{1,0:T(8,128)(2,1)} collective-permute-done((bf16[1280,3072]{1,0:T(8,128)(2,1)}, bf16[1280,3072]{1,0:T(8,128)(2,1)}, u32[]{:S(2)}, u32[]{:S(2)}) %collective-permute-start.44) | collective-permute-done | bytes 7864352 | tf_op jit(solution)/shard_map/ppermute | solution.py:774
  647.3 12.2 %add_convert_fusion = bf16[1280,3072]{1,0:T(8,128)(2,1)} fusion(bf16[1280,3072]{1,0:T(8,128)(2,1)} %collective-permute-done.44, bf16[1280,3072]{1,0:T(8,128)(2,1)} %get-tuple-element.82), kind=kLoop, calls=%fused_computation | loop fusion | flops 15728640 | bytes 23592960 | tf_op jit(solution)/shard_map/convert_element_type | solution.py:778
  661.0 13.6 %shard_map.175.refs_2_ = f32[1024,2560]{1,0:T(8,128)} custom-call(bf16[1024,896]{1,0:T(8,128)(2,1)S(1)} %copy-done.5, bf16[2560,2688]{1,0:T(8,128)(2,1)} %all-gather.3.cloned.1.call-done.refs_2_.refs_1_), custom_call_target="tpu_custom_call" | custom-call | flops 4697620480 | bytes 24248320 | tf_op jit(solution)/shard_map/pallas_call | solution.py:630
  674.6 14.3 %shard_map.176 = (bf16[2,512,640]{2,1,0:T(8,128)(2,1)}, bf16[2,512,640]{2,1,0:T(8,128)(2,1)}, bf16[2,512,640]{2,1,0:T(8,128)(2,1)S(1)}, bf16[2,512,640]{2,1,0:T(8,128)(2,1)S(1)}) custom-call(s32[1]{0:T(128)} %bitcast.me_ref, bf16[1024,1024]{1,0:T(8,128)(2,1)} %get-tuple-element.84.hidden_ref.refs_0_, ...), custom_call_target="tpu_custom_call" | custom-call | flops 5368709120 | bytes 23068672 | tf_op jit(solution)/shard_map/pallas_call | solution.py:671
  692.9 9.9 %shard_map.179 = (bf16[2,512,640]{2,1,0:T(8,128)(2,1)}, bf16[2,512,640]{2,1,0:T(8,128)(2,1)S(1)}, bf16[2,512,640]{2,1,0:T(8,128)(2,1)S(1)}, bf16[2,512,640]{2,1,0:T(8,128)(2,1)S(1)}) custom-call(s32[1]{0:T(128)} %bitcast.me_ref, bf16[1024,768]{1,0:T(8,128)(2,1)} %bitcast.35.refs_0_, bf16[2560,1408]{1,0:T(8,128)(2,1)} %get-tuple-element.64.refs_1_.weight_ref.refs_0_), custom_call_target="tpu_custom_call" | custom-call | flops 4026531840 | bytes 14024704 | tf_op jit(solution)/shard_map/pallas_call | solution.py:671
  709.6 39.7 %collective-permute-done.34 = f32[4,256]{1,0:T(4,128)S(1)} collective-permute-done((f32[4,256]{1,0:T(4,128)S(1)}, f32[4,256]{1,0:T(4,128)S(1)}, u32[]{:S(2)}, u32[]{:S(2)}) %collective-permute-start.34) | collective-permute-done | bytes 4128 | tf_op jit(solution)/shard_map/ppermute | solution.py:38
  749.6 3.8 collective-permute-done.37
  754.9 2.1 collective-permute-done.35
  757.0 5.5 collective-permute-done.38
  777.6 9.9 %collective-permute-done.27 = bf16[512,640]{1,0:T(8,128)(2,1)} collective-permute-done((bf16[512,640]{1,0:T(8,128)(2,1)S(1)}, bf16[512,640]{1,0:T(8,128)(2,1)}, u32[]{:S(2)}, u32[]{:S(2)}) %collective-permute-start.27) | collective-permute-done | bytes 655392 | tf_op jit(solution)/shard_map/ppermute | solution.py:38
  790.7 8.9 collective-permute-done.31
  802.9 3.1 fusion.22
  808.4 3.9 reduce-scatter.6.cloned.1.call-done
  812.3 3.2 fusion.74
  815.5 135.7 %reduce-scatter.8.cloned.1.call-done = bf16[320,3072]{1,0:T(8,128)(2,1)} async-done(((bf16[1280,3072]{1,0:T(8,128)(2,1)}), bf16[320,3072]{1,0:T(8,128)(2,1)}) %reduce-scatter.8.cloned.1.call-update) | async-done | bytes 1966096 | tf_op jit(solution)/shard_map/reduce_scatter | solution.py:783
  953.8 2.9 fusion.26
  (313 shorter events, 119.9 us)
Async XLA Ops:
  7.2 268.6 %all-gather.3.cloned.1.call-start = ((), (), s32[]{:S(2)}) async-start(), calls=%async_computation.7 | async-start | bytes 15482880 | tf_op jit(solution)/shard_map/all_gather | solution.py:770
  82.8 267.4 %all-gather.5.cloned.1.call-start = ((), (), s32[]{:S(2)}) async-start(), calls=%async_computation.8 | async-start | bytes 17694720 | tf_op jit(solution)/shard_map/all_gather | solution.py:770
  92.6 23.9 %all-to-all-start = ((bf16[4,256,768]{2,1,0:T(8,128)(2,1)}), bf16[4,256,768]{2,1,0:T(8,128)(2,1)S(1)}, u32[]{:S(2)}, u32[]{:S(2)}) async-start(bf16[4,256,768]{2,1,0:T(8,128)(2,1)} %bitcast.4), calls=%async_computation | async-start | bytes 3145728 | tf_op jit(solution)/shard_map/all_to_all | solution.py:144
  119.1 7.8 collective-permute-start
  120.6 7.9 collective-permute-start.1
  126.9 5.0 collective-permute-start.2
  129.4 5.0 collective-permute-start.3
  172.3 27.1 %collective-permute-start.4 = (bf16[2,512,640]{2,1,0:T(8,128)(2,1)S(1)}, bf16[2,512,640]{2,1,0:T(8,128)(2,1)S(1)}, u32[]{:S(2)}, u32[]{:S(2)}) collective-permute-start(bf16[2,512,640]{2,1,0:T(8,128)(2,1)S(1)} %get-tuple-element.67), channel_id=1, source_target_pairs={{0,1},{1,0},{2,3},{3,2},{4,5},{5,4},{6,7},{7,6},{8,9},{9,8},{10,11... | collective-permute-start | bytes 3932168 | tf_op jit(solution)/shard_map/ppermute | solution.py:38
  173.3 28.6 %collective-permute-start.6 = (bf16[2,512,640]{2,1,0:T(8,128)(2,1)S(1)}, bf16[2,512,640]{2,1,0:T(8,128)(2,1)S(1)}, u32[]{:S(2)}, u32[]{:S(2)}) collective-permute-start(bf16[2,512,640]{2,1,0:T(8,128)(2,1)S(1)} %get-tuple-element.69), channel_id=1, source_target_pairs={{0,2},{1,3},{2,0},{3,1},{4,6},{5,7},{6,4},{7,5},{8,10},{9,11},{10,... | collective-permute-start | bytes 3932168 | tf_op jit(solution)/shard_map/ppermute | solution.py:38
  200.5 13.9 %collective-permute-start.5 = (bf16[512,640]{1,0:T(8,128)(2,1)}, bf16[512,640]{1,0:T(8,128)(2,1)S(1)}, u32[]{:S(2)}, u32[]{:S(2)}) collective-permute-start(bf16[512,640]{1,0:T(8,128)(2,1)} %fusion.34), channel_id=1, source_target_pairs={{0,2},{1,3},{2,0},{3,1},{4,6},{5,7},{6,4},{7,5},{8,10},{9,11},{10,... | collective-permute-start | bytes 1966088 | tf_op jit(solution)/shard_map/ppermute | solution.py:38
  203.9 12.6 %collective-permute-start.7 = (bf16[512,640]{1,0:T(8,128)(2,1)}, bf16[512,640]{1,0:T(8,128)(2,1)}, u32[]{:S(2)}, u32[]{:S(2)}) collective-permute-start(bf16[512,640]{1,0:T(8,128)(2,1)} %fusion.35), channel_id=1, source_target_pairs={{0,1},{1,0},{2,3},{3,2},{4,5},{5,4},{6,7},{7,6},{8,9},{9,8},{10,11... | collective-permute-start | bytes 1966088 | tf_op jit(solution)/shard_map/ppermute | solution.py:38
  218.0 245.4 %copy-start.27 = (f32[512,640]{1,0:T(8,128)}, f32[512,640]{1,0:T(8,128)S(1)}, u32[]{:S(2)}) copy-start(f32[512,640]{1,0:T(8,128)S(1)} %bitcast_add_fusion.6) | copy-start | bytes 3932164
  222.4 26.7 %collective-permute-start.8 = (bf16[1024,640]{1,0:T(8,128)(2,1)S(1)}, bf16[1024,640]{1,0:T(8,128)(2,1)S(1)}, u32[]{:S(2)}, u32[]{:S(2)}) collective-permute-start(bf16[1024,640]{1,0:T(8,128)(2,1)S(1)} %get-tuple-element.120), channel_id=1, source_target_pairs={{0,1},{1,0},{2,3},{3,2},{4,5},{5,4},{6,7},{7,6},{8,9},{9,8},{10,11... | collective-permute-start | bytes 3932168 | tf_op jit(solution)/shard_map/ppermute | solution.py:38
  223.5 27.7 %collective-permute-start.9 = (bf16[1024,640]{1,0:T(8,128)(2,1)S(1)}, bf16[1024,640]{1,0:T(8,128)(2,1)S(1)}, u32[]{:S(2)}, u32[]{:S(2)}) collective-permute-start(bf16[1024,640]{1,0:T(8,128)(2,1)S(1)} %get-tuple-element.120), channel_id=1, source_target_pairs={{0,2},{1,3},{2,0},{3,1},{4,6},{5,7},{6,4},{7,5},{8,10},{9,11},{10,... | collective-permute-start | bytes 3932168 | tf_op jit(solution)/shard_map/ppermute | solution.py:38
  250.0 13.3 %collective-permute-start.10 = (bf16[512,640]{1,0:T(8,128)(2,1)}, bf16[512,640]{1,0:T(8,128)(2,1)S(1)}, u32[]{:S(2)}, u32[]{:S(2)}) collective-permute-start(bf16[512,640]{1,0:T(8,128)(2,1)} %slice.278), channel_id=1, source_target_pairs={{0,2},{1,3},{2,0},{3,1},{4,6},{5,7},{6,4},{7,5},{8,10},{9,11},{10,... | collective-permute-start | bytes 1966088 | tf_op jit(solution)/shard_map/ppermute | solution.py:38
  253.1 11.2 %collective-permute-start.11 = (bf16[512,640]{1,0:T(8,128)(2,1)}, bf16[512,640]{1,0:T(8,128)(2,1)}, u32[]{:S(2)}, u32[]{:S(2)}) collective-permute-start(bf16[512,640]{1,0:T(8,128)(2,1)} %slice.279), channel_id=1, source_target_pairs={{0,1},{1,0},{2,3},{3,2},{4,5},{5,4},{6,7},{7,6},{8,9},{9,8},{10,11... | collective-permute-start | bytes 1966088 | tf_op jit(solution)/shard_map/ppermute | solution.py:38
  382.8 55.0 %copy-start.23 = (bf16[1024,1024]{1,0:T(8,128)(2,1)S(1)}, bf16[1024,1024]{1,0:T(8,128)(2,1)}, u32[]{:S(2)}) copy-start(bf16[1024,1024]{1,0:T(8,128)(2,1)} %get-tuple-element.125.refs_1_.d_up_ref) | copy-start | bytes 6291460
  401.6 36.3 %copy-start.22 = (bf16[1024,1024]{1,0:T(8,128)(2,1)S(1)}, bf16[1024,1024]{1,0:T(8,128)(2,1)}, u32[]{:S(2)}) copy-start(bf16[1024,1024]{1,0:T(8,128)(2,1)} %get-tuple-element.121.refs_0_.d_gate_ref) | copy-start | bytes 6291460
  401.6 32.8 %collective-permute-start.14 = (bf16[2,512,640]{2,1,0:T(8,128)(2,1)S(1)}, bf16[2,512,640]{2,1,0:T(8,128)(2,1)S(1)}, u32[]{:S(2)}, u32[]{:S(2)}) collective-permute-start(bf16[2,512,640]{2,1,0:T(8,128)(2,1)S(1)} %get-tuple-element.79), channel_id=1, source_target_pairs={{0,2},{1,3},{2,0},{3,1},{4,6},{5,7},{6,4},{7,5},{8,10},{9,11},{10,... | collective-permute-start | bytes 3932168 | tf_op jit(solution)/shard_map/ppermute | solution.py:38
  403.1 33.0 %collective-permute-start.12 = (bf16[2,512,640]{2,1,0:T(8,128)(2,1)S(1)}, bf16[2,512,640]{2,1,0:T(8,128)(2,1)S(1)}, u32[]{:S(2)}, u32[]{:S(2)}) collective-permute-start(bf16[2,512,640]{2,1,0:T(8,128)(2,1)S(1)} %get-tuple-element.77), channel_id=1, source_target_pairs={{0,1},{1,0},{2,3},{3,2},{4,5},{5,4},{6,7},{7,6},{8,9},{9,8},{10,11... | collective-permute-start | bytes 3932168 | tf_op jit(solution)/shard_map/ppermute | solution.py:38
  404.6 29.3 %collective-permute-start.16 = (f32[8,128]{1,0:T(8,128)S(1)}, f32[8,128]{1,0:T(8,128)S(1)}, u32[]{:S(2)}, u32[]{:S(2)}) collective-permute-start(f32[8,128]{1,0:T(8,128)S(1)} %add_bitcast_fusion), channel_id=1, source_target_pairs={{0,1},{1,0},{2,3},{3,2},{4,5},{5,4},{6,7},{7,6},{8,9},{9,8},{10,11... | collective-permute-start | bytes 12296 | tf_op jit(solution)/shard_map/ppermute | solution.py:38
  433.9 29.0 %collective-permute-start.17 = (f32[8,128]{1,0:T(8,128)S(1)}, f32[8,128]{1,0:T(8,128)S(1)}, u32[]{:S(2)}, u32[]{:S(2)}) collective-permute-start(f32[8,128]{1,0:T(8,128)S(1)} %fusion.82), channel_id=1, source_target_pairs={{0,2},{1,3},{2,0},{3,1},{4,6},{5,7},{6,4},{7,5},{8,10},{9,11},{10,... | collective-permute-start | bytes 12296 | tf_op jit(solution)/shard_map/ppermute | solution.py:38
  434.6 28.3 %collective-permute-start.15 = (bf16[512,640]{1,0:T(8,128)(2,1)S(1)}, bf16[512,640]{1,0:T(8,128)(2,1)S(1)}, u32[]{:S(2)}, u32[]{:S(2)}) collective-permute-start(bf16[512,640]{1,0:T(8,128)(2,1)S(1)} %fusion.37), channel_id=1, source_target_pairs={{0,1},{1,0},{2,3},{3,2},{4,5},{5,4},{6,7},{7,6},{8,9},{9,8},{10,11... | collective-permute-start | bytes 1966088 | tf_op jit(solution)/shard_map/ppermute | solution.py:38
  436.3 26.8 %collective-permute-start.13 = (bf16[512,640]{1,0:T(8,128)(2,1)S(1)}, bf16[512,640]{1,0:T(8,128)(2,1)S(1)}, u32[]{:S(2)}, u32[]{:S(2)}) collective-permute-start(bf16[512,640]{1,0:T(8,128)(2,1)S(1)} %fusion.36), channel_id=1, source_target_pairs={{0,2},{1,3},{2,0},{3,1},{4,6},{5,7},{6,4},{7,5},{8,10},{9,11},{10,... | collective-permute-start | bytes 1966088 | tf_op jit(solution)/shard_map/ppermute | solution.py:38
  463.1 49.2 %slice-start = ((s8[7208960]{0:T(1024)(128)(4,1)}), s8[4194304]{0:T(1024)(128)(4,1)S(1)}, s32[]{:S(2)}) async-start(s8[7208960]{0:T(1024)(128)(4,1)} %bitcast.127), calls=%async_computation.12 | async-start | bytes 8388608
  464.8 47.5 %slice-start.1 = ((s8[7208960]{0:T(1024)(128)(4,1)}), s8[3014656]{0:T(1024)(128)(4,1)S(1)}, s32[]{:S(2)}) async-start(s8[7208960]{0:T(1024)(128)(4,1)} %bitcast.127), calls=%async_computation.13 | async-start | bytes 6029312
  468.8 28.9 %collective-permute-start.19 = (bf16[1024,640]{1,0:T(8,128)(2,1)S(1)}, bf16[1024,640]{1,0:T(8,128)(2,1)S(1)}, u32[]{:S(2)}, u32[]{:S(2)}) collective-permute-start(bf16[1024,640]{1,0:T(8,128)(2,1)S(1)} %get-tuple-element.83.own), channel_id=1, source_target_pairs={{0,2},{1,3},{2,0},{3,1},{4,6},{5,7},{6,4},{7,5},{8,10},{9,11},{10,... | collective-permute-start | bytes 3932168 | tf_op jit(solution)/shard_map/ppermute | solution.py:38
  469.4 29.1 %collective-permute-start.18 = (bf16[1024,640]{1,0:T(8,128)(2,1)S(1)}, bf16[1024,640]{1,0:T(8,128)(2,1)S(1)}, u32[]{:S(2)}, u32[]{:S(2)}) collective-permute-start(bf16[1024,640]{1,0:T(8,128)(2,1)S(1)} %get-tuple-element.83.own), channel_id=1, source_target_pairs={{0,1},{1,0},{2,3},{3,2},{4,5},{5,4},{6,7},{7,6},{8,9},{9,8},{10,11... | collective-permute-start | bytes 3932168 | tf_op jit(solution)/shard_map/ppermute | solution.py:38
  497.8 14.3 %collective-permute-start.21 = (bf16[512,640]{1,0:T(8,128)(2,1)S(1)}, bf16[512,640]{1,0:T(8,128)(2,1)S(1)}, u32[]{:S(2)}, u32[]{:S(2)}) collective-permute-start(bf16[512,640]{1,0:T(8,128)(2,1)S(1)} %slice.291), channel_id=1, source_target_pairs={{0,1},{1,0},{2,3},{3,2},{4,5},{5,4},{6,7},{7,6},{8,9},{9,8},{10,11... | collective-permute-start | bytes 1966088 | tf_op jit(solution)/shard_map/ppermute | solution.py:38
  498.5 13.8 %collective-permute-start.20 = (bf16[512,640]{1,0:T(8,128)(2,1)S(1)}, bf16[512,640]{1,0:T(8,128)(2,1)S(1)}, u32[]{:S(2)}, u32[]{:S(2)}) collective-permute-start(bf16[512,640]{1,0:T(8,128)(2,1)S(1)} %slice.290), channel_id=1, source_target_pairs={{0,2},{1,3},{2,0},{3,1},{4,6},{5,7},{6,4},{7,5},{8,10},{9,11},{10,... | collective-permute-start | bytes 1966088 | tf_op jit(solution)/shard_map/ppermute | solution.py:38
  518.8 18.5 %all-to-all-start.2 = ((bf16[4,256,640]{2,1,0:T(8,128)(2,1)}), bf16[4,256,640]{2,1,0:T(8,128)(2,1)}, u32[]{:S(2)}, u32[]{:S(2)}) async-start(bf16[4,256,640]{2,1,0:T(8,128)(2,1)} %bitcast.22), calls=%async_computation.2 | async-start | bytes 2621440 | tf_op jit(solution)/shard_map/all_to_all | solution.py:144
  560.1 8.0 collective-permute-start.23
  562.3 6.9 collective-permute-start.25
  568.9 5.3 collective-permute-start.24
  576.1 5.3 collective-permute-start.26
  585.7 20.7 %all-to-all-start.3 = ((bf16[256,4,768]{2,0,1:T(8,128)(2,1)}), bf16[256,4,768]{2,0,1:T(8,128)(2,1)}, u32[]{:S(2)}, u32[]{:S(2)}) async-start(bf16[256,4,768]{2,0,1:T(8,128)(2,1)} %bitcast.136), calls=%async_computation.3 | async-start | bytes 3145728 | tf_op jit(solution)/shard_map/all_to_all | solution.py:148
  590.0 216.0 %reduce-scatter.4.cloned.1.call-start = ((), (), s32[]{:S(2)}) async-start(), calls=%async_computation.9 | async-start | bytes 4505600 | tf_op jit(solution)/shard_map/reduce_scatter | solution.py:783
  590.1 34.2 %collective-permute-start.43 = (bf16[1280,2688]{1,0:T(8,128)(2,1)}, bf16[1280,2688]{1,0:T(8,128)(2,1)}, u32[]{:S(2)}, u32[]{:S(2)}) collective-permute-start(bf16[1280,2688]{1,0:T(8,128)(2,1)} %get-tuple-element.113), channel_id=1, source_target_pairs={{0,4},{4,0},{8,12},{12,8},{16,20},{20,16},{24,28},{28,24},{1,5},{5... | collective-permute-start | bytes 20643848 | tf_op jit(solution)/shard_map/ppermute | solution.py:774
  601.6 15.8 %collective-permute-start.42 = (bf16[1280,640]{1,0:T(8,128)(2,1)}, bf16[1280,640]{1,0:T(8,128)(2,1)S(1)}, u32[]{:S(2)}, u32[]{:S(2)}) collective-permute-start(bf16[1280,640]{1,0:T(8,128)(2,1)} %get-tuple-element.111), channel_id=1, source_target_pairs={{0,4},{4,0},{8,12},{12,8},{16,20},{20,16},{24,28},{28,24},{1,5},{5... | collective-permute-start | bytes 4915208 | tf_op jit(solution)/shard_map/ppermute | solution.py:774
  617.4 4.2 collective-permute-start.41
  624.1 188.2 %reduce-scatter.6.cloned.1.call-start = ((), (), s32[]{:S(2)}) async-start(), calls=%async_computation.10 | async-start | bytes 8601600 | tf_op jit(solution)/shard_map/reduce_scatter | solution.py:783
  634.4 316.7 %reduce-scatter.8.cloned.1.call-start = ((), (), s32[]{:S(2)}) async-start(), calls=%async_computation.11 | async-start | bytes 9830400 | tf_op jit(solution)/shard_map/reduce_scatter | solution.py:783
  634.5 12.8 %collective-permute-start.44 = (bf16[1280,3072]{1,0:T(8,128)(2,1)}, bf16[1280,3072]{1,0:T(8,128)(2,1)}, u32[]{:S(2)}, u32[]{:S(2)}) collective-permute-start(bf16[1280,3072]{1,0:T(8,128)(2,1)} %get-tuple-element.114), channel_id=1, source_target_pairs={{0,4},{4,0},{8,12},{12,8},{16,20},{20,16},{24,28},{28,24},{1,5},{5... | collective-permute-start | bytes 23592968 | tf_op jit(solution)/shard_map/ppermute | solution.py:774
  690.0 73.9 %collective-permute-start.22 = (bf16[2,512,640]{2,1,0:T(8,128)(2,1)}, bf16[2,512,640]{2,1,0:T(8,128)(2,1)}, u32[]{:S(2)}, u32[]{:S(2)}) collective-permute-start(bf16[2,512,640]{2,1,0:T(8,128)(2,1)} %get-tuple-element.91), channel_id=1, source_target_pairs={{0,1},{1,0},{2,3},{3,2},{4,5},{5,4},{6,7},{7,6},{8,9},{9,8},{10,11... | collective-permute-start | bytes 3932168 | tf_op jit(solution)/shard_map/ppermute | solution.py:38
  691.4 76.3 %collective-permute-start.28 = (bf16[2,512,640]{2,1,0:T(8,128)(2,1)}, bf16[2,512,640]{2,1,0:T(8,128)(2,1)}, u32[]{:S(2)}, u32[]{:S(2)}) collective-permute-start(bf16[2,512,640]{2,1,0:T(8,128)(2,1)} %get-tuple-element.97), channel_id=1, source_target_pairs={{0,2},{1,3},{2,0},{3,1},{4,6},{5,7},{6,4},{7,5},{8,10},{9,11},{10,... | collective-permute-start | bytes 3932168 | tf_op jit(solution)/shard_map/ppermute | solution.py:38
  692.8 62.1 %copy-start.59 = (bf16[320]{0:T(512)(128)(2,1)S(1)}, bf16[320]{0:T(512)(128)(2,1)}, u32[]{:S(2)}) copy-start(bf16[320]{0:T(512)(128)(2,1)} %param.15) | copy-start | bytes 1924
  692.8 62.1 %copy-start.56 = (bf16[320]{0:T(512)(128)(2,1)S(1)}, bf16[320]{0:T(512)(128)(2,1)}, u32[]{:S(2)}) copy-start(bf16[320]{0:T(512)(128)(2,1)} %param.12) | copy-start | bytes 1924
  692.8 71.2 %copy-start.8 = (bf16[2,512,640]{2,1,0:T(8,128)(2,1)S(1)}, bf16[2,512,640]{2,1,0:T(8,128)(2,1)}, u32[]{:S(2)}) copy-start(bf16[2,512,640]{2,1,0:T(8,128)(2,1)} %copy-done.7) | copy-start | bytes 3932164
  692.8 15.3 %collective-permute-start.36 = (f32[8,320]{1,0:T(8,128)S(1)}, f32[8,320]{1,0:T(8,128)S(1)}, u32[]{:S(2)}, u32[]{:S(2)}) collective-permute-start(f32[8,320]{1,0:T(8,128)S(1)} %reshape.217), channel_id=1, source_target_pairs={{0,4},{4,0},{8,12},{12,8},{16,20},{20,16},{24,28},{28,24},{1,5},{5... | collective-permute-start | bytes 30728 | tf_op jit(solution)/shard_map/ppermute | solution.py:138
  705.9 66.6 %collective-permute-start.30 = (bf16[2,512,640]{2,1,0:T(8,128)(2,1)}, bf16[2,512,640]{2,1,0:T(8,128)(2,1)}, u32[]{:S(2)}, u32[]{:S(2)}) collective-permute-start(bf16[2,512,640]{2,1,0:T(8,128)(2,1)} %get-tuple-element.103), channel_id=1, source_target_pairs={{0,1},{1,0},{2,3},{3,2},{4,5},{5,4},{6,7},{7,6},{8,9},{9,8},{10,11... | collective-permute-start | bytes 3932168 | tf_op jit(solution)/shard_map/ppermute | solution.py:38
  707.6 41.7 %collective-permute-start.34 = (f32[4,256]{1,0:T(4,128)S(1)}, f32[4,256]{1,0:T(4,128)S(1)}, u32[]{:S(2)}, u32[]{:S(2)}) collective-permute-start(f32[4,256]{1,0:T(4,128)S(1)} %dynamic_update_slice.45), channel_id=1, source_target_pairs={{0,1},{1,0},{2,3},{3,2},{4,5},{5,4},{6,7},{7,6},{8,9},{9,8},{10,11... | collective-permute-start | bytes 12296 | tf_op jit(solution)/shard_map/ppermute | solution.py:38
  708.1 67.6 %collective-permute-start.32 = (bf16[2,512,640]{2,1,0:T(8,128)(2,1)}, bf16[2,512,640]{2,1,0:T(8,128)(2,1)}, u32[]{:S(2)}, u32[]{:S(2)}) collective-permute-start(bf16[2,512,640]{2,1,0:T(8,128)(2,1)} %copy-done.20), channel_id=1, source_target_pairs={{0,2},{1,3},{2,0},{3,1},{4,6},{5,7},{6,4},{7,5},{8,10},{9,11},{10,... | collective-permute-start | bytes 3932168 | tf_op jit(solution)/shard_map/ppermute | solution.py:38
  749.3 4.1 collective-permute-start.37
  753.4 3.6 collective-permute-start.35
  757.0 5.5 collective-permute-start.38
  762.5 3.7 collective-permute-start.39
  766.2 5.6 collective-permute-start.40
  769.8 17.7 %collective-permute-start.27 = (bf16[512,640]{1,0:T(8,128)(2,1)S(1)}, bf16[512,640]{1,0:T(8,128)(2,1)}, u32[]{:S(2)}, u32[]{:S(2)}) collective-permute-start(bf16[512,640]{1,0:T(8,128)(2,1)S(1)} %fusion.38), channel_id=1, source_target_pairs={{0,2},{1,3},{2,0},{3,1},{4,6},{5,7},{6,4},{7,5},{8,10},{9,11},{10,... | collective-permute-start | bytes 1966088 | tf_op jit(solution)/shard_map/ppermute | solution.py:38
  770.3 18.7 %collective-permute-start.29 = (bf16[512,640]{1,0:T(8,128)(2,1)}, bf16[512,640]{1,0:T(8,128)(2,1)}, u32[]{:S(2)}, u32[]{:S(2)}) collective-permute-start(bf16[512,640]{1,0:T(8,128)(2,1)} %fusion.39), channel_id=1, source_target_pairs={{0,1},{1,0},{2,3},{3,2},{4,5},{5,4},{6,7},{7,6},{8,9},{9,8},{10,11... | collective-permute-start | bytes 1966088 | tf_op jit(solution)/shard_map/ppermute | solution.py:38
  774.0 25.5 %collective-permute-start.31 = (bf16[512,640]{1,0:T(8,128)(2,1)S(1)}, bf16[512,640]{1,0:T(8,128)(2,1)S(1)}, u32[]{:S(2)}, u32[]{:S(2)}) collective-permute-start(bf16[512,640]{1,0:T(8,128)(2,1)S(1)} %fusion.40), channel_id=1, source_target_pairs={{0,2},{1,3},{2,0},{3,1},{4,6},{5,7},{6,4},{7,5},{8,10},{9,11},{10,... | collective-permute-start | bytes 1966088 | tf_op jit(solution)/shard_map/ppermute | solution.py:38
  777.1 23.9 %collective-permute-start.33 = (bf16[512,640]{1,0:T(8,128)(2,1)S(1)}, bf16[512,640]{1,0:T(8,128)(2,1)S(1)}, u32[]{:S(2)}, u32[]{:S(2)}) collective-permute-start(bf16[512,640]{1,0:T(8,128)(2,1)S(1)} %fusion.41), channel_id=1, source_target_pairs={{0,1},{1,0},{2,3},{3,2},{4,5},{5,4},{6,7},{7,6},{8,9},{9,8},{10,11... | collective-permute-start | bytes 1966088 | tf_op jit(solution)/shard_map/ppermute | solution.py:38
  815.5 137.8 %copy-start.39 = (bf16[320,1920]{1,0:T(8,128)(2,1)S(1)}, bf16[320,1920]{1,0:T(8,128)(2,1)}, u32[]{:S(2)}) copy-start(bf16[320,1920]{1,0:T(8,128)(2,1)} %refs_0_.1) | copy-start | bytes 3686404
  956.7 3.6 collective-permute-start.45
  960.3 3.6 collective-permute-start.46
  (58 other events, 558.6 us)
Sparse Core Ops, SparseCore 0:
  82.9 124.8 all-gather.2
  209.5 140.6 all-gather.4
  624.2 64.7 reduce-scatter.3
  691.2 121.0 reduce-scatter.5
  814.4 136.7 reduce-scatter.7

commit v10 on v8

--- a/solution.py
+++ b/solution.py
@@ -544,19 +544,47 @@
     )(core_index(), rows, above, d_gate, d_up, hidden)
 
 
-def pieces_grad_kernel(me_ref, core_ref, own, along_x, along_y, top, bottom, right_ref, kept, sent):
+def hold_piece(pieces, held):
+    *blocks, top, bottom = pieces
     at = pl.program_id(0)
-    half = top.shape[0]
-    for index, piece in enumerate((own, along_x, along_y)):
+    for index, piece in enumerate(blocks):
 
         @pl.when(at == index)
         def _(piece=piece):
-            keep_half(core_ref, tn(piece[...], right_ref[...]).astype(BF16), kept, sent)
-
-    @pl.when(at == 3)
+            held[...] = piece[...]
+
+    @pl.when(at == len(blocks))
     def _():
-        total = tn(top[...], right_ref[:half]) + tn(bottom[...], right_ref[half:])
-        keep_half(core_ref, total.astype(BF16), kept, sent)
+        half = top.shape[0]
+        held[:half] = top[...]
+        held[half:] = bottom[...]
+
+
+def pieces_grad_kernel(me_ref, core_ref, *refs):
+    *pieces, right_ref, kept, sent, held = refs
+    hold_piece(pieces, held)
+    keep_half(core_ref, tn(held[...], right_ref[...]).astype(BF16), kept, sent)
+
+
+def add_kernel(left_ref, right_ref, out_ref):
+    out_ref[...] = (left_ref[...].astype(F32) + right_ref[...].astype(F32)).astype(BF16)
+
+
+def add_pair(left, right):
+    rows, cols = left.shape
+    if rows % 256 or cols % 128:
+        return (left.astype(F32) + right.astype(F32)).astype(BF16)
+    steps = 10 if rows % 160 == 0 else 8
+    spec = pl.BlockSpec((rows // steps, cols), lambda at: (at, 0))
+    return pl.pallas_call(
+        add_kernel,
+        grid=(steps,),
+        out_shape=jax.ShapeDtypeStruct(left.shape, BF16),
+        in_specs=[spec, spec],
+        out_specs=spec,
+        compiler_params=in_order(16),
+        cost_estimate=cost(rows * cols, 6 * rows * cols),
+    )(left, right)
 
 
 def pieces_grad(pieces, right):
@@ -577,6 +605,7 @@
                 pl.BlockSpec((step // 2, cols), lambda at, me_ref, core_ref: (me_ref[0] ^ at, 0))
             ]
             * 2,
+            scratch_shapes=[pltpu.VMEM((tokens, step), BF16)],
         ),
         out_shape=(out, out),
         compiler_params=in_order(48),
@@ -660,25 +689,17 @@
     )(me, *lefts, weight, *partial)
 
 
-def pieces_kernel(start, me_ref, own, along_x, along_y, top, bottom, weight_ref, out_ref, total):
+def pieces_kernel(start, me_ref, *refs):
+    *pieces, weight_ref, out_ref, total, held = refs
+    hold_piece(pieces, held)
     at = pl.program_id(0)
-    width = out_ref.shape[1]
-    half = top.shape[0]
-    for index, piece in enumerate((own, along_x, along_y)):
-
-        @pl.when(at == index)
-        def _(index=index, piece=piece):
-            part = nn(piece[...], weight_ref[:, start : start + width])
-            if index:
-                total[...] += part
-            else:
-                total[...] = part
+    part = nn(held[...], weight_ref[:, start : start + out_ref.shape[1]])
+    part = part + jnp.where(at > 0, total[...], 0.0)
+    total[...] = part
 
     @pl.when(at == 3)
     def _():
-        weight = weight_ref[:, start : start + width]
-        out_ref[:half] = (total[:half] + nn(top[...], weight)).astype(BF16)
-        out_ref[half:] = (total[half:] + nn(bottom[...], weight)).astype(BF16)
+        out_ref[...] = part.astype(BF16)
 
 
 def pieces_product(pieces, weight, start, width):
@@ -693,7 +714,7 @@
             in_specs=[pl.BlockSpec(piece.shape, lambda at, me_ref: (0, 0)) for piece in pieces]
             + [pl.BlockSpec((step, cols), lambda at, me_ref: (me_ref[0] ^ at, 0))],
             out_specs=pl.BlockSpec((tokens, width), lambda at, me_ref: (0, 0)),
-            scratch_shapes=[pltpu.VMEM((tokens, width), F32)],
+            scratch_shapes=[pltpu.VMEM((tokens, width), F32), pltpu.VMEM((tokens, step), BF16)],
         ),
         out_shape=jax.ShapeDtypeStruct((tokens, width), BF16),
         compiler_params=in_order(40),
@@ -748,7 +769,7 @@
         kept, sent = local
         count = lax.axis_size("tok")
         got = lax.ppermute(sent, "tok", [(i, i ^ 1) for i in range(count)])
-        both = (kept.astype(F32) + got.astype(F32)).astype(BF16)
+        both = add_pair(kept, got)
         groups = [list(range(core, count, 2)) for core in range(2)]
         total = lax.psum_scatter(
             both, "tok", scatter_dimension=0, tiled=True, axis_index_groups=groups

time: 896 us -> 900 us (level)
  other arithmetic: 100 us -> 71.6 us
  Pallas kernels: 247 us -> 267 us
  local copies, waits for them, and re-layouts: 37.3 us -> 50.6 us
    convert_element_type x4 -> x0, other arithmetic: 28.3 us -> none  [pair_to_tok(): both = (kept.astype(F32) + got.astype(F32)).astype(BF16)]
    pallas_call x0 -> x4, Pallas kernels: none -> 19.1 us  [add_pair(): pl.pallas_call(add_kernel, grid=(steps,), out_shape=jax.ShapeDtypeStruct(...]
    ppermute x40, waiting for transfers between devices: 218 us -> 203 us  [swap(): return lax.ppermute(block, 'mdl', [(i, i ^ distance) for i in range(size)])]
    unnamed x135 -> x151, local copies, waits for them, and re-layouts: 14.7 us -> 27.7 us
  transfers between devices with their start and end apart: 56 -> 56, of which waited for: 32 -> 30; matrix products, arithmetic and copies ran while one was open for 17% -> 13% of each run, Pallas kernels for 18% -> 20%
where the time goes in v10:
time: 900 us; the launch traced here: 892 us
  waiting for transfers between devices  340 us (38%)
  Pallas kernels  267 us (30%)
  other arithmetic  71.6 us (8%)
  matrix products  68.6 us (8%)
  starting transfers between devices  60.3 us (7%)
  local copies, waits for them, and re-layouts  50.6 us (6%)
  blocking collectives  18.4 us (2%)
  between operations  15.3 us (2%)
    ppermute x40, waiting for transfers between devices, swap(): return lax.ppermute(block, 'mdl', [(i, i ^ distance) for i in range(size)])  203 us
    pallas_call x1, Pallas kernels, first_gather(): pl.pallas_call(functools.partial(first_kernel, parts), out_shape=[jax.Sha...  70.2 us
    dot_general x7, matrix products, nn(): return jnp.dot(left_op, right_op, preferred_element_type=F32)  68.6 us
    reduce_scatter x4, waiting for transfers between devices, pair_to_tok(): lax.psum_scatter(both, 'tok', scatter_dimension=0, tiled=True, axis_index...  65.6 us
    pallas_call x4, Pallas kernels, scatter_product(): pl.pallas_call(functools.partial(payload_kernel, starts), grid_spec=pltpu...  49.9 us
    pallas_call x2, Pallas kernels, part_grad(): pl.pallas_call(part_kernel, grid=(pairs,), out_shape=(out, out), in_specs...  48.5 us
    ppermute x40, starting transfers between devices, swap(): return lax.ppermute(block, 'mdl', [(i, i ^ distance) for i in range(size)])  46.4 us
    all_to_all x2, waiting for transfers between devices, rows_to_cols(): return lax.all_to_all(block, 'mdl', split_axis=0, concat_axis=1, tiled=True)  35.1 us
  transfers between devices with their start and end apart: 56, of which 30 were waited for; matrix products, arithmetic and copies ran while one was open for 13% of the time, Pallas kernels for 20%

profile of v10, /device:TPU:0, one launch (start us, length us, event | category | flops | bytes accessed | tf_op | source)
XLA Modules:
  0.0 891.9 jit_solution(4159277852467408879)
XLA Ops:
  12.5 70.2 %shard_map.169 = (bf16[1024,2560]{1,0:T(8,128)(2,1)}, bf16[2560,1408]{1,0:T(8,128)(2,1)}, bf16[320,2688]{1,0:T(8,128)(2,1)}, bf16[320,3072]{1,0:T(8,128)(2,1)}) custom-call(bf16[1024,640]{1,0:T(8,128)(2,1)} %x_ref.1, bf16[320,1408]{1,0:T(8,128)(2,1)} %pad_maximum_fusion.3.w_ref, f32[320,1]{1,0:T(8,128)} %reshape.224.gain_ref, bf16[320,1920]{1,0:T(8,128)(2,1)} %refs_0_.1, ...), custom_call_target="tpu_custom_call" | custom-call | tf_op jit(solution)/shard_map/pallas_call | solution.py:296
  83.5 9.0 %fusion.30 = bf16[1024,768]{1,0:T(8,128)(2,1)} fusion(bf16[1024,2560]{1,0:T(8,128)(2,1)} %get-tuple-element.91.left_ref, bf16[2560,1408]{1,0:T(8,128)(2,1)} %get-tuple-element.60.refs_1_.refs_5_.refs_0_), kind=kOutput, calls=%fused_computation.57 | convolution fusion | flops 4027318272 | bytes 10747904 | tf_op jit(solution)/shard_map/dot_general | solution.py:33
  92.6 4.1 all-to-all-start
  98.4 18.1 %all-to-all-done = bf16[4,256,768]{2,1,0:T(8,128)(2,1)S(1)} async-done(((bf16[4,256,768]{2,1,0:T(8,128)(2,1)}), bf16[4,256,768]{2,1,0:T(8,128)(2,1)S(1)}, u32[]{:S(2)}, u32[]{:S(2)}) %all-to-all-start) | async-done | bytes 1572896 | tf_op jit(solution)/shard_map/all_to_all | solution.py:144
  121.5 5.5 collective-permute-done
  134.4 11.2 %att_f.1 = (bf16[256,2560]{1,0:T(8,128)(2,1)S(1)}, f32[10,256,1]{2,1,0:T(8,128)S(1)}) custom-call(s32[1]{0:T(128)} %bitcast.1.first_ref, bf16[256,3072]{1,0:T(8,128)(2,1)S(1)} %bitcast.129, bf16[1024,512]{1,0:T(8,128)(2,1)S(1)} %constant_dynamic-update-slice_fusion.4.kv_ref, f32[256,128]{1,0:T(8,128)S(1)} %get-tuple-element.145.cos_ref, ...), custom_call_target="tpu_custom_call" | custom-call | flops 2684354560 | bytes 3670016 | tf_op jit(solution)/shard_map/att_f/pallas_call | solution.py:393
  145.8 18.4 %all_to_all.76 = bf16[256,4,640]{2,0,1:T(8,128)(2,1)} all-to-all(bf16[256,4,640]{2,0,1:T(8,128)(2,1)S(1)} %bitcast.138), channel_id=1, replica_groups=mesh['tok'=8,'mdl'=4] {'mdl'}, dimensions={1} | all-to-all | bytes 2621440 | tf_op jit(solution)/shard_map/all_to_all | solution.py:148
  164.2 7.8 shard_map.170
  173.7 25.5 %collective-permute-done.4 = bf16[2,512,640]{2,1,0:T(8,128)(2,1)S(1)} collective-permute-done((bf16[2,512,640]{2,1,0:T(8,128)(2,1)S(1)}, bf16[2,512,640]{2,1,0:T(8,128)(2,1)S(1)}, u32[]{:S(2)}, u32[]{:S(2)}) %collective-permute-start.4) | collective-permute-done | bytes 1310752 | tf_op jit(solution)/shard_map/ppermute | solution.py:38
  204.2 10.1 %collective-permute-done.5 = bf16[512,640]{1,0:T(8,128)(2,1)S(1)} collective-permute-done((bf16[512,640]{1,0:T(8,128)(2,1)}, bf16[512,640]{1,0:T(8,128)(2,1)S(1)}, u32[]{:S(2)}, u32[]{:S(2)}) %collective-permute-start.5) | collective-permute-done | bytes 655392 | tf_op jit(solution)/shard_map/ppermute | solution.py:38
  218.0 2.9 broadcast_in_dim.31
  225.3 24.1 %collective-permute-done.8 = bf16[1024,640]{1,0:T(8,128)(2,1)S(1)} collective-permute-done((bf16[1024,640]{1,0:T(8,128)(2,1)S(1)}, bf16[1024,640]{1,0:T(8,128)(2,1)S(1)}, u32[]{:S(2)}, u32[]{:S(2)}) %collective-permute-start.8) | collective-permute-done | bytes 1310752 | tf_op jit(solution)/shard_map/ppermute | solution.py:38
  258.7 5.0 collective-permute-done.10
  266.7 3.7 fusion
  270.4 5.7 fusion.1.rows_ref
  276.2 9.6 %fusion.12 = f32[896,1024]{0,1:T(8,128)S(1)} fusion(bf16[1024,2560]{1,0:T(8,128)(2,1)} %above_ref.2, bf16[2560,2688]{1,0:T(8,128)(2,1)} %all-gather.3.cloned.1.call-done.refs_2_.refs_1_), kind=kOutput, calls=%fused_computation.15 | convolution fusion | flops 4697620480 | bytes 13500416 | tf_op jit(solution)/shard_map/dot_general | solution.py:33
  285.7 8.0 fusion.8
  293.7 9.3 %add_reduce_fusion.1 = (f32[1024]{0:T(1024)S(1)}, bf16[1024,896]{1,0:T(8,128)(2,1)S(1)}, bf16[1024,896]{1,0:T(8,128)(2,1)S(1)}, bf16[1024,896]{1,0:T(8,128)(2,1)S(1)}) fusion(f32[1024,896]{1,0:T(8,128)S(1)} %fusion.8, f32[896,1024]{0,1:T(8,128)S(1)} %fusion.12, bf16[1024,2560]{1,0:T(8,128)(2,1)S(1)} %copy-done.46, ...), kind=kOutput, calls=%fused_computation.29 | convolution fusion | flops 4723309568 | bytes 22679552 | tf_op jit(solution)/shard_map/dot_general | solution.py:33
  303.1 23.5 %shard_map.171 = (bf16[1280,2688]{1,0:T(8,128)(2,1)}, bf16[1280,2688]{1,0:T(8,128)(2,1)}) custom-call(s32[1]{0:T(128)} %bitcast.14.core_ref, bf16[1024,2560]{1,0:T(8,128)(2,1)} %fusion.1.rows_ref, bf16[1024,2560]{1,0:T(8,128)(2,1)} %above_ref.2, bf16[1024,896]{1,0:T(8,128)(2,1)S(1)} %get-tuple-element.71.d_gate_ref.refs_0_, ...), custom_call_target="tpu_custom_call" | custom-call | flops 14092861440 | bytes 29753344 | tf_op jit(solution)/shard_map/pallas_call | solution.py:533
  326.6 15.3 %shard_map.172.refs_3_ = f32[1024,2560]{1,0:T(8,128)} custom-call(bf16[1024,896]{1,0:T(8,128)(2,1)S(1)} %get-tuple-element.71.d_gate_ref.refs_0_, bf16[1024,896]{1,0:T(8,128)(2,1)S(1)} %get-tuple-element.119.d_up_ref.refs_1_, bf16[2560,2688]{1,0:T(8,128)(2,1)} %all-gather.3.cloned.1.call-done.refs_2_.refs_1_), custom_call_target="tpu_custom_call" | custom-call | flops 9395240960 | bytes 24248320 | tf_op jit(solution)/shard_map/pallas_call | solution.py:634
  341.9 8.3 all-gather.5.cloned.1.call-done.refs_2_.refs_1_
  350.2 10.7 %fusion.2 = f32[1024,1024]{1,0:T(8,128)} fusion(bf16[1024,2560]{1,0:T(8,128)(2,1)} %above_ref.2, bf16[2560,3072]{1,0:T(8,128)(2,1)} %all-gather.5.cloned.1.call-done.refs_2_.refs_1_), kind=kOutput, calls=%fused_computation.5 | convolution fusion | flops 5368709120 | bytes 14680064 | tf_op jit(solution)/shard_map/dot_general | solution.py:33
  360.9 8.9 %fusion.4 = f32[1024,1024]{1,0:T(8,128)} fusion(bf16[1024,2560]{1,0:T(8,128)(2,1)} %fusion.1.rows_ref, bf16[2560,3072]{1,0:T(8,128)(2,1)S(1)} %copy-done.42), kind=kOutput, calls=%fused_computation.7 | convolution fusion | flops 5368709120 | bytes 14680064 | tf_op jit(solution)/shard_map/dot_general | solution.py:33
  369.8 13.0 %fusion.67 = (bf16[1024,1024]{1,0:T(8,128)(2,1)}, f32[1024]{0:T(1024)S(1)}, bf16[1024,1024]{1,0:T(8,128)(2,1)}, bf16[1024,1024]{1,0:T(8,128)(2,1)}) fusion(f32[1024,1024]{1,0:T(8,128)} %fusion.2, f32[1024,1024]{1,0:T(8,128)} %fusion.4, bf16[1024,2560]{1,0:T(8,128)(2,1)S(1)} %bitcast.137, bf16[2560,3072]{1,0:T(8,128)(2,1)S(1)} %copy-done.42), kind=kOutput, calls=%fused_computation.158 | convolution fusion | flops 5398068224 | bytes 25169920 | tf_op jit(solution)/shard_map/dot_general | solution.py:33
  382.8 18.7 %shard_map.173 = (bf16[2,512,640]{2,1,0:T(8,128)(2,1)S(1)}, bf16[2,512,640]{2,1,0:T(8,128)(2,1)S(1)}, bf16[2,512,640]{2,1,0:T(8,128)(2,1)S(1)}, bf16[2,512,640]{2,1,0:T(8,128)(2,1)S(1)}) custom-call(s32[1]{0:T(128)} %bitcast.me_ref, bf16[1024,1024]{1,0:T(8,128)(2,1)} %get-tuple-element.113.refs_0_.d_gate_ref, ...), custom_call_target="tpu_custom_call" | custom-call | flops 10737418240 | bytes 25165824 | tf_op jit(solution)/shard_map/pallas_call | solution.py:675
  405.1 28.7 %collective-permute-done.16 = f32[8,128]{1,0:T(8,128)S(1)} collective-permute-done((f32[8,128]{1,0:T(8,128)S(1)}, f32[8,128]{1,0:T(8,128)S(1)}, u32[]{:S(2)}, u32[]{:S(2)}) %collective-permute-start.16) | collective-permute-done | bytes 4128 | tf_op jit(solution)/shard_map/ppermute | solution.py:38
  438.7 24.9 %shard_map.174 = (bf16[1280,3072]{1,0:T(8,128)(2,1)}, bf16[1280,3072]{1,0:T(8,128)(2,1)}) custom-call(s32[1]{0:T(128)} %bitcast.14.core_ref, bf16[1024,2560]{1,0:T(8,128)(2,1)} %fusion.1.rows_ref, bf16[1024,2560]{1,0:T(8,128)(2,1)} %above_ref.2, bf16[1024,1024]{1,0:T(8,128)(2,1)S(1)} %copy-done.31, bf16[1024,1024]{1,0:T(8,128)(2,1)S(1)} %copy-done.32, ...), custom_call_target="tpu_custom_call" | custom-call | flops 16106127360 | bytes 32505856 | tf_op jit(solution)/shard_map/pallas_call | solution.py:533
  466.6 3.9 fusion.70
  471.9 27.6 %collective-permute-done.20.refs_2_ = bf16[1024,640]{1,0:T(8,128)(2,1)S(1)} collective-permute-done((bf16[1024,640]{1,0:T(8,128)(2,1)S(1)}, bf16[1024,640]{1,0:T(8,128)(2,1)S(1)}, u32[]{:S(2)}, u32[]{:S(2)}) %collective-permute-start.20) | collective-permute-done | bytes 1310752 | tf_op jit(solution)/shard_map/ppermute | solution.py:38
  502.4 11.4 %collective-permute-done.22.refs_4_ = bf16[512,640]{1,0:T(8,128)(2,1)S(1)} collective-permute-done((bf16[512,640]{1,0:T(8,128)(2,1)S(1)}, bf16[512,640]{1,0:T(8,128)(2,1)S(1)}, u32[]{:S(2)}, u32[]{:S(2)}) %collective-permute-start.22) | collective-permute-done | bytes 655392 | tf_op jit(solution)/shard_map/ppermute | solution.py:38
  514.8 6.9 shard_map.177
  521.8 8.0 shard_map.181
  529.8 3.7 collective-permute-done.42.right_ref
  534.9 3.6 shard_map.182
  538.6 3.0 copy-done.3
  541.6 6.8 shard_map.183
  551.5 12.5 %collective-permute-done.44.right_ref = bf16[1280,3072]{1,0:T(8,128)(2,1)S(1)} collective-permute-done((bf16[1280,3072]{1,0:T(8,128)(2,1)}, bf16[1280,3072]{1,0:T(8,128)(2,1)S(1)}, u32[]{:S(2)}, u32[]{:S(2)}) %collective-permute-start.44) | collective-permute-done | bytes 7864352 | tf_op jit(solution)/shard_map/ppermute | solution.py:771
  564.0 3.3 copy-done.2
  569.2 3.1 copy-done
  572.3 4.8 all-to-all-start.2
  577.1 17.1 %all-to-all-done.2 = bf16[4,256,640]{2,1,0:T(8,128)(2,1)} async-done(((bf16[4,256,640]{2,1,0:T(8,128)(2,1)}), bf16[4,256,640]{2,1,0:T(8,128)(2,1)}, u32[]{:S(2)}, u32[]{:S(2)}) %all-to-all-start.2) | async-done | bytes 1310752 | tf_op jit(solution)/shard_map/all_to_all | solution.py:144
  598.5 15.6 %att_b.1 = (bf16[256,2560]{1,0:T(8,128)(2,1)S(1)}, f32[1024,512]{1,0:T(8,128)S(1)}) custom-call(s32[1]{0:T(128)} %bitcast.1.first_ref, bf16[256,3072]{1,0:T(8,128)(2,1)S(1)} %bitcast.130, bf16[1024,512]{1,0:T(8,128)(2,1)S(1)} %copy-done.19, f32[256,128]{1,0:T(8,128)S(1)} %copy-done.27, f32[256,128]{1,0:T(8,128)S(1)} %copy-done.25, s32[256,1]{1,0:T(8,128)S(1)} %copy-done.21, ...), custom_call_target="tpu_custom_call" | custom-call | flops 6710886400 | bytes 8388608 | tf_op jit(solution)/shard_map/att_b/pallas_call | solution.py:419
  617.2 4.8 collective-permute-done.23
  624.2 3.7 collective-permute-done.24
  631.1 3.8 collective-permute-done.26
  639.2 4.3 all-to-all-start.3
  643.6 3.7 multiply_reduce_fusion
  647.3 13.5 %shard_map.175.refs_2_ = f32[1024,2560]{1,0:T(8,128)} custom-call(bf16[1024,896]{1,0:T(8,128)(2,1)S(1)} %get-tuple-element.81.hidden_ref.refs_0_, bf16[2560,2688]{1,0:T(8,128)(2,1)} %all-gather.3.cloned.1.call-done.refs_2_.refs_1_), custom_call_target="tpu_custom_call" | custom-call | flops 4697620480 | bytes 24248320 | tf_op jit(solution)/shard_map/pallas_call | solution.py:634
  660.8 14.1 %shard_map.176 = (bf16[2,512,640]{2,1,0:T(8,128)(2,1)}, bf16[2,512,640]{2,1,0:T(8,128)(2,1)}, bf16[2,512,640]{2,1,0:T(8,128)(2,1)S(1)}, bf16[2,512,640]{2,1,0:T(8,128)(2,1)S(1)}) custom-call(s32[1]{0:T(128)} %bitcast.me_ref, bf16[1024,1024]{1,0:T(8,128)(2,1)} %get-tuple-element.80.hidden_ref.refs_0_, ...), custom_call_target="tpu_custom_call" | custom-call | flops 5368709120 | bytes 23068672 | tf_op jit(solution)/shard_map/pallas_call | solution.py:675
  679.0 9.3 %shard_map.178 = (bf16[2,512,640]{2,1,0:T(8,128)(2,1)S(1)}, bf16[2,512,640]{2,1,0:T(8,128)(2,1)}, bf16[2,512,640]{2,1,0:T(8,128)(2,1)S(1)}, bf16[2,512,640]{2,1,0:T(8,128)(2,1)S(1)}) custom-call(s32[1]{0:T(128)} %bitcast.me_ref, bf16[1024,768]{1,0:T(8,128)(2,1)} %bitcast.35.refs_0_, bf16[2560,1408]{1,0:T(8,128)(2,1)} %get-tuple-element.60.refs_1_.refs_5_.refs_0_), custom_call_target="tpu_custom_call" | custom-call | flops 4026531840 | bytes 14024704 | tf_op jit(solution)/shard_map/pallas_call | solution.py:675
  692.7 9.2 %shard_map.179 = (bf16[1280,768]{1,0:T(8,128)(2,1)S(1)}, bf16[1280,768]{1,0:T(8,128)(2,1)}, f32[2560,1]{1,0:T(8,128)S(1)}) custom-call(s32[1]{0:T(128)} %bitcast.14.core_ref, bf16[1024,2560]{1,0:T(8,128)(2,1)} %get-tuple-element.91.left_ref, bf16[1024,768]{1,0:T(8,128)(2,1)S(1)} %multiply_convert_fusion.2.right_ref, ...), custom_call_target="tpu_custom_call" | custom-call | flops 4026531840 | bytes 10747904 | tf_op jit(solution)/shard_map/pallas_call | solution.py:500
  708.9 3.1 collective-permute-done.37
  715.8 7.2 collective-permute-done.38
  724.5 9.4 %collective-permute-done.28 = bf16[2,512,640]{2,1,0:T(8,128)(2,1)} collective-permute-done((bf16[2,512,640]{2,1,0:T(8,128)(2,1)}, bf16[2,512,640]{2,1,0:T(8,128)(2,1)}, u32[]{:S(2)}, u32[]{:S(2)}) %collective-permute-start.28) | collective-permute-done | bytes 1310752 | tf_op jit(solution)/shard_map/ppermute | solution.py:38
  736.0 7.3 collective-permute-done.39
  744.8 6.8 shard_map.180
  751.7 10.0 %collective-permute-done.35 = f32[4,256]{1,0:T(4,128)S(1)} collective-permute-done((f32[4,256]{1,0:T(4,128)S(1)}, f32[4,256]{1,0:T(4,128)S(1)}, u32[]{:S(2)}, u32[]{:S(2)}) %collective-permute-start.35) | collective-permute-done | bytes 4128 | tf_op jit(solution)/shard_map/ppermute | solution.py:38
  769.3 10.3 %collective-permute-done.27 = bf16[512,640]{1,0:T(8,128)(2,1)} collective-permute-done((bf16[512,640]{1,0:T(8,128)(2,1)}, bf16[512,640]{1,0:T(8,128)(2,1)}, u32[]{:S(2)}, u32[]{:S(2)}) %collective-permute-start.27) | collective-permute-done | bytes 655392 | tf_op jit(solution)/shard_map/ppermute | solution.py:38
  782.6 10.6 %collective-permute-done.33 = bf16[512,640]{1,0:T(8,128)(2,1)S(1)} collective-permute-done((bf16[512,640]{1,0:T(8,128)(2,1)S(1)}, bf16[512,640]{1,0:T(8,128)(2,1)S(1)}, u32[]{:S(2)}, u32[]{:S(2)}) %collective-permute-start.33) | collective-permute-done | bytes 655392 | tf_op jit(solution)/shard_map/ppermute | solution.py:38
  796.8 3.2 fusion.22
  801.9 3.2 fusion.74
  805.2 27.8 %reduce-scatter.11.cloned.1.call-done = bf16[320,3072]{1,0:T(8,128)(2,1)} async-done(((bf16[1280,3072]{1,0:T(8,128)(2,1)}), bf16[320,3072]{1,0:T(8,128)(2,1)}) %reduce-scatter.11.cloned.1.call-update) | async-done | bytes 1966096 | tf_op jit(solution)/shard_map/reduce_scatter | solution.py:774
  835.5 2.9 fusion.26
  839.9 37.8 %reduce-scatter.5.cloned.1.call-done = bf16[320,768]{1,0:T(8,128)(2,1)} async-done(((bf16[1280,768]{1,0:T(8,128)(2,1)}), bf16[320,768]{1,0:T(8,128)(2,1)}) %reduce-scatter.5.cloned.1.call-update) | async-done | bytes 491536 | tf_op jit(solution)/shard_map/reduce_scatter | solution.py:774
  (331 shorter events, 139.0 us)
Async XLA Ops:
  7.2 269.0 %all-gather.3.cloned.1.call-start = ((), (), s32[]{:S(2)}) async-start(), calls=%async_computation.8 | async-start | bytes 15482880 | tf_op jit(solution)/shard_map/all_gather | solution.py:766
  82.8 267.4 %all-gather.5.cloned.1.call-start = ((), (), s32[]{:S(2)}) async-start(), calls=%async_computation.9 | async-start | bytes 17694720 | tf_op jit(solution)/shard_map/all_gather | solution.py:766
  92.6 23.9 %all-to-all-start = ((bf16[4,256,768]{2,1,0:T(8,128)(2,1)}), bf16[4,256,768]{2,1,0:T(8,128)(2,1)S(1)}, u32[]{:S(2)}, u32[]{:S(2)}) async-start(bf16[4,256,768]{2,1,0:T(8,128)(2,1)} %bitcast.4), calls=%async_computation | async-start | bytes 3145728 | tf_op jit(solution)/shard_map/all_to_all | solution.py:144
  96.7 703.3 %reduce-scatter.7.cloned.1.call-start = ((), (), s32[]{:S(2)}) async-start(), calls=%async_computation.11 | async-start | bytes 2048000 | tf_op jit(solution)/shard_map/reduce_scatter | solution.py:774
  118.3 27.3 %copy-start.24 = (f32[256,128]{1,0:T(8,128)}, f32[256,128]{1,0:T(8,128)S(1)}, u32[]{:S(2)}) copy-start(f32[256,128]{1,0:T(8,128)S(1)} %get-tuple-element.144.sin_ref) | copy-start | bytes 393220
  119.2 7.8 collective-permute-start
  120.6 7.9 collective-permute-start.1
  126.9 5.0 collective-permute-start.2
  129.4 5.0 collective-permute-start.3
  172.1 27.2 %collective-permute-start.4 = (bf16[2,512,640]{2,1,0:T(8,128)(2,1)S(1)}, bf16[2,512,640]{2,1,0:T(8,128)(2,1)S(1)}, u32[]{:S(2)}, u32[]{:S(2)}) collective-permute-start(bf16[2,512,640]{2,1,0:T(8,128)(2,1)S(1)} %get-tuple-element.63), channel_id=1, source_target_pairs={{0,1},{1,0},{2,3},{3,2},{4,5},{5,4},{6,7},{7,6},{8,9},{9,8},{10,11... | collective-permute-start | bytes 3932168 | tf_op jit(solution)/shard_map/ppermute | solution.py:38
  173.1 28.6 %collective-permute-start.6 = (bf16[2,512,640]{2,1,0:T(8,128)(2,1)S(1)}, bf16[2,512,640]{2,1,0:T(8,128)(2,1)S(1)}, u32[]{:S(2)}, u32[]{:S(2)}) collective-permute-start(bf16[2,512,640]{2,1,0:T(8,128)(2,1)S(1)} %get-tuple-element.65), channel_id=1, source_target_pairs={{0,2},{1,3},{2,0},{3,1},{4,6},{5,7},{6,4},{7,5},{8,10},{9,11},{10,... | collective-permute-start | bytes 3932168 | tf_op jit(solution)/shard_map/ppermute | solution.py:38
  200.4 13.9 %collective-permute-start.5 = (bf16[512,640]{1,0:T(8,128)(2,1)}, bf16[512,640]{1,0:T(8,128)(2,1)S(1)}, u32[]{:S(2)}, u32[]{:S(2)}) collective-permute-start(bf16[512,640]{1,0:T(8,128)(2,1)} %fusion.34), channel_id=1, source_target_pairs={{0,2},{1,3},{2,0},{3,1},{4,6},{5,7},{6,4},{7,5},{8,10},{9,11},{10,... | collective-permute-start | bytes 1966088 | tf_op jit(solution)/shard_map/ppermute | solution.py:38
  203.7 12.7 %collective-permute-start.7 = (bf16[512,640]{1,0:T(8,128)(2,1)}, bf16[512,640]{1,0:T(8,128)(2,1)}, u32[]{:S(2)}, u32[]{:S(2)}) collective-permute-start(bf16[512,640]{1,0:T(8,128)(2,1)} %fusion.35), channel_id=1, source_target_pairs={{0,1},{1,0},{2,3},{3,2},{4,5},{5,4},{6,7},{7,6},{8,9},{9,8},{10,11... | collective-permute-start | bytes 1966088 | tf_op jit(solution)/shard_map/ppermute | solution.py:38
  222.6 26.8 %collective-permute-start.8 = (bf16[1024,640]{1,0:T(8,128)(2,1)S(1)}, bf16[1024,640]{1,0:T(8,128)(2,1)S(1)}, u32[]{:S(2)}, u32[]{:S(2)}) collective-permute-start(bf16[1024,640]{1,0:T(8,128)(2,1)S(1)} %get-tuple-element.112), channel_id=1, source_target_pairs={{0,1},{1,0},{2,3},{3,2},{4,5},{5,4},{6,7},{7,6},{8,9},{9,8},{10,11... | collective-permute-start | bytes 3932168 | tf_op jit(solution)/shard_map/ppermute | solution.py:38
  223.8 27.7 %collective-permute-start.9 = (bf16[1024,640]{1,0:T(8,128)(2,1)S(1)}, bf16[1024,640]{1,0:T(8,128)(2,1)S(1)}, u32[]{:S(2)}, u32[]{:S(2)}) collective-permute-start(bf16[1024,640]{1,0:T(8,128)(2,1)S(1)} %get-tuple-element.112), channel_id=1, source_target_pairs={{0,2},{1,3},{2,0},{3,1},{4,6},{5,7},{6,4},{7,5},{8,10},{9,11},{10,... | collective-permute-start | bytes 3932168 | tf_op jit(solution)/shard_map/ppermute | solution.py:38
  250.3 13.4 %collective-permute-start.10 = (bf16[512,640]{1,0:T(8,128)(2,1)}, bf16[512,640]{1,0:T(8,128)(2,1)S(1)}, u32[]{:S(2)}, u32[]{:S(2)}) collective-permute-start(bf16[512,640]{1,0:T(8,128)(2,1)} %slice.270), channel_id=1, source_target_pairs={{0,2},{1,3},{2,0},{3,1},{4,6},{5,7},{6,4},{7,5},{8,10},{9,11},{10,... | collective-permute-start | bytes 1966088 | tf_op jit(solution)/shard_map/ppermute | solution.py:38
  253.5 11.2 %collective-permute-start.11 = (bf16[512,640]{1,0:T(8,128)(2,1)}, bf16[512,640]{1,0:T(8,128)(2,1)}, u32[]{:S(2)}, u32[]{:S(2)}) collective-permute-start(bf16[512,640]{1,0:T(8,128)(2,1)} %slice.271), channel_id=1, source_target_pairs={{0,1},{1,0},{2,3},{3,2},{4,5},{5,4},{6,7},{7,6},{8,9},{9,8},{10,11... | collective-permute-start | bytes 1966088 | tf_op jit(solution)/shard_map/ppermute | solution.py:38
  382.8 55.9 %copy-start.32 = (bf16[1024,1024]{1,0:T(8,128)(2,1)S(1)}, bf16[1024,1024]{1,0:T(8,128)(2,1)}, u32[]{:S(2)}) copy-start(bf16[1024,1024]{1,0:T(8,128)(2,1)} %get-tuple-element.117.refs_1_.d_up_ref) | copy-start | bytes 6291460
  401.5 37.2 %copy-start.31 = (bf16[1024,1024]{1,0:T(8,128)(2,1)S(1)}, bf16[1024,1024]{1,0:T(8,128)(2,1)}, u32[]{:S(2)}) copy-start(bf16[1024,1024]{1,0:T(8,128)(2,1)} %get-tuple-element.113.refs_0_.d_gate_ref) | copy-start | bytes 6291460
  401.6 32.8 %collective-permute-start.14 = (bf16[2,512,640]{2,1,0:T(8,128)(2,1)S(1)}, bf16[2,512,640]{2,1,0:T(8,128)(2,1)S(1)}, u32[]{:S(2)}, u32[]{:S(2)}) collective-permute-start(bf16[2,512,640]{2,1,0:T(8,128)(2,1)S(1)} %get-tuple-element.75), channel_id=1, source_target_pairs={{0,2},{1,3},{2,0},{3,1},{4,6},{5,7},{6,4},{7,5},{8,10},{9,11},{10,... | collective-permute-start | bytes 3932168 | tf_op jit(solution)/shard_map/ppermute | solution.py:38
  403.1 33.0 %collective-permute-start.12 = (bf16[2,512,640]{2,1,0:T(8,128)(2,1)S(1)}, bf16[2,512,640]{2,1,0:T(8,128)(2,1)S(1)}, u32[]{:S(2)}, u32[]{:S(2)}) collective-permute-start(bf16[2,512,640]{2,1,0:T(8,128)(2,1)S(1)} %get-tuple-element.73), channel_id=1, source_target_pairs={{0,1},{1,0},{2,3},{3,2},{4,5},{5,4},{6,7},{7,6},{8,9},{9,8},{10,11... | collective-permute-start | bytes 3932168 | tf_op jit(solution)/shard_map/ppermute | solution.py:38
  404.6 29.3 %collective-permute-start.16 = (f32[8,128]{1,0:T(8,128)S(1)}, f32[8,128]{1,0:T(8,128)S(1)}, u32[]{:S(2)}, u32[]{:S(2)}) collective-permute-start(f32[8,128]{1,0:T(8,128)S(1)} %add_bitcast_fusion), channel_id=1, source_target_pairs={{0,1},{1,0},{2,3},{3,2},{4,5},{5,4},{6,7},{7,6},{8,9},{9,8},{10,11... | collective-permute-start | bytes 12296 | tf_op jit(solution)/shard_map/ppermute | solution.py:38
  433.8 29.8 %collective-permute-start.17 = (f32[8,128]{1,0:T(8,128)S(1)}, f32[8,128]{1,0:T(8,128)S(1)}, u32[]{:S(2)}, u32[]{:S(2)}) collective-permute-start(f32[8,128]{1,0:T(8,128)S(1)} %fusion.82), channel_id=1, source_target_pairs={{0,2},{1,3},{2,0},{3,1},{4,6},{5,7},{6,4},{7,5},{8,10},{9,11},{10,... | collective-permute-start | bytes 12296 | tf_op jit(solution)/shard_map/ppermute | solution.py:38
  434.6 29.1 %collective-permute-start.15 = (bf16[512,640]{1,0:T(8,128)(2,1)S(1)}, bf16[512,640]{1,0:T(8,128)(2,1)S(1)}, u32[]{:S(2)}, u32[]{:S(2)}) collective-permute-start(bf16[512,640]{1,0:T(8,128)(2,1)S(1)} %fusion.37), channel_id=1, source_target_pairs={{0,1},{1,0},{2,3},{3,2},{4,5},{5,4},{6,7},{7,6},{8,9},{9,8},{10,11... | collective-permute-start | bytes 1966088 | tf_op jit(solution)/shard_map/ppermute | solution.py:38
  436.1 27.6 %copy-start.54 = (bf16[2,512,640]{2,1,0:T(8,128)(2,1)}, bf16[2,512,640]{2,1,0:T(8,128)(2,1)S(1)}, u32[]{:S(2)}) copy-start(bf16[2,512,640]{2,1,0:T(8,128)(2,1)S(1)} %collective-permute-done.12) | copy-start | bytes 3932164
  437.3 26.7 %collective-permute-start.13 = (bf16[512,640]{1,0:T(8,128)(2,1)}, bf16[512,640]{1,0:T(8,128)(2,1)}, u32[]{:S(2)}, u32[]{:S(2)}) collective-permute-start(bf16[512,640]{1,0:T(8,128)(2,1)} %fusion.36), channel_id=1, source_target_pairs={{0,2},{1,3},{2,0},{3,1},{4,6},{5,7},{6,4},{7,5},{8,10},{9,11},{10,... | collective-permute-start | bytes 1966088 | tf_op jit(solution)/shard_map/ppermute | solution.py:38
  465.0 49.8 %slice-start = ((s8[7208960]{0:T(1024)(128)(4,1)}), s8[4194304]{0:T(1024)(128)(4,1)S(1)}, s32[]{:S(2)}) async-start(s8[7208960]{0:T(1024)(128)(4,1)} %bitcast.126), calls=%async_computation.14 | async-start | bytes 8388608
  466.6 48.2 %slice-start.1 = ((s8[7208960]{0:T(1024)(128)(4,1)}), s8[3014656]{0:T(1024)(128)(4,1)S(1)}, s32[]{:S(2)}) async-start(s8[7208960]{0:T(1024)(128)(4,1)} %bitcast.126), calls=%async_computation.15 | async-start | bytes 6029312
  470.5 28.9 %collective-permute-start.20 = (bf16[1024,640]{1,0:T(8,128)(2,1)S(1)}, bf16[1024,640]{1,0:T(8,128)(2,1)S(1)}, u32[]{:S(2)}, u32[]{:S(2)}) collective-permute-start(bf16[1024,640]{1,0:T(8,128)(2,1)S(1)} %get-tuple-element.79.refs_0_), channel_id=1, source_target_pairs={{0,2},{1,3},{2,0},{3,1},{4,6},{5,7},{6,4},{7,5},{8,10},{9,11},{10,... | collective-permute-start | bytes 3932168 | tf_op jit(solution)/shard_map/ppermute | solution.py:38
  471.1 29.6 %collective-permute-start.19 = (bf16[1024,640]{1,0:T(8,128)(2,1)S(1)}, bf16[1024,640]{1,0:T(8,128)(2,1)S(1)}, u32[]{:S(2)}, u32[]{:S(2)}) collective-permute-start(bf16[1024,640]{1,0:T(8,128)(2,1)S(1)} %get-tuple-element.79.refs_0_), channel_id=1, source_target_pairs={{0,1},{1,0},{2,3},{3,2},{4,5},{5,4},{6,7},{7,6},{8,9},{9,8},{10,11... | collective-permute-start | bytes 3932168 | tf_op jit(solution)/shard_map/ppermute | solution.py:38
  471.9 66.7 %collective-permute-start.43 = (bf16[1280,2688]{1,0:T(8,128)(2,1)}, bf16[1280,2688]{1,0:T(8,128)(2,1)}, u32[]{:S(2)}, u32[]{:S(2)}) collective-permute-start(bf16[1280,2688]{1,0:T(8,128)(2,1)} %get-tuple-element.105), channel_id=1, source_target_pairs={{0,4},{4,0},{8,12},{12,8},{16,20},{20,16},{24,28},{28,24},{1,5},{5... | collective-permute-start | bytes 20643848 | tf_op jit(solution)/shard_map/ppermute | solution.py:771
  499.5 14.3 %collective-permute-start.22 = (bf16[512,640]{1,0:T(8,128)(2,1)S(1)}, bf16[512,640]{1,0:T(8,128)(2,1)S(1)}, u32[]{:S(2)}, u32[]{:S(2)}) collective-permute-start(bf16[512,640]{1,0:T(8,128)(2,1)S(1)} %slice.285), channel_id=1, source_target_pairs={{0,1},{1,0},{2,3},{3,2},{4,5},{5,4},{6,7},{7,6},{8,9},{9,8},{10,11... | collective-permute-start | bytes 1966088 | tf_op jit(solution)/shard_map/ppermute | solution.py:38
  500.7 14.1 %collective-permute-start.21 = (bf16[512,640]{1,0:T(8,128)(2,1)S(1)}, bf16[512,640]{1,0:T(8,128)(2,1)S(1)}, u32[]{:S(2)}, u32[]{:S(2)}) collective-permute-start(bf16[512,640]{1,0:T(8,128)(2,1)S(1)} %slice.284), channel_id=1, source_target_pairs={{0,2},{1,3},{2,0},{3,1},{4,6},{5,7},{6,4},{7,5},{8,10},{9,11},{10,... | collective-permute-start | bytes 1966088 | tf_op jit(solution)/shard_map/ppermute | solution.py:38
  529.8 3.7 collective-permute-start.42
  538.5 263.4 %reduce-scatter.9.cloned.1.call-start = ((), (), s32[]{:S(2)}) async-start(), calls=%async_computation.12 | async-start | bytes 8601600 | tf_op jit(solution)/shard_map/reduce_scatter | solution.py:774
  551.3 281.7 %reduce-scatter.11.cloned.1.call-start = ((), (), s32[]{:S(2)}) async-start(), calls=%async_computation.13 | async-start | bytes 9830400 | tf_op jit(solution)/shard_map/reduce_scatter | solution.py:774
  551.3 12.7 %collective-permute-start.44 = (bf16[1280,3072]{1,0:T(8,128)(2,1)}, bf16[1280,3072]{1,0:T(8,128)(2,1)S(1)}, u32[]{:S(2)}, u32[]{:S(2)}) collective-permute-start(bf16[1280,3072]{1,0:T(8,128)(2,1)} %get-tuple-element.106), channel_id=1, source_target_pairs={{0,4},{4,0},{8,12},{12,8},{16,20},{20,16},{24,28},{28,24},{1,5},{5... | collective-permute-start | bytes 23592968 | tf_op jit(solution)/shard_map/ppermute | solution.py:771
  572.3 21.9 %all-to-all-start.2 = ((bf16[4,256,640]{2,1,0:T(8,128)(2,1)}), bf16[4,256,640]{2,1,0:T(8,128)(2,1)}, u32[]{:S(2)}, u32[]{:S(2)}) async-start(bf16[4,256,640]{2,1,0:T(8,128)(2,1)} %bitcast.24), calls=%async_computation.2 | async-start | bytes 2621440 | tf_op jit(solution)/shard_map/all_to_all | solution.py:144
  614.4 7.6 collective-permute-start.23
  616.6 7.5 collective-permute-start.25
  622.7 5.2 collective-permute-start.24
  629.7 5.2 collective-permute-start.26
  639.2 39.8 %all-to-all-start.3 = ((bf16[256,4,768]{2,0,1:T(8,128)(2,1)}), bf16[256,4,768]{2,0,1:T(8,128)(2,1)}, u32[]{:S(2)}, u32[]{:S(2)}) async-start(bf16[256,4,768]{2,0,1:T(8,128)(2,1)} %bitcast.124), calls=%async_computation.3 | async-start | bytes 3145728 | tf_op jit(solution)/shard_map/all_to_all | solution.py:148
  643.5 234.2 %reduce-scatter.5.cloned.1.call-start = ((), (), s32[]{:S(2)}) async-start(), calls=%async_computation.10 | async-start | bytes 2457600 | tf_op jit(solution)/shard_map/reduce_scatter | solution.py:774
  677.1 30.8 %collective-permute-start.18 = (bf16[2,512,640]{2,1,0:T(8,128)(2,1)}, bf16[2,512,640]{2,1,0:T(8,128)(2,1)}, u32[]{:S(2)}, u32[]{:S(2)}) collective-permute-start(bf16[2,512,640]{2,1,0:T(8,128)(2,1)} %get-tuple-element.83), channel_id=1, source_target_pairs={{0,1},{1,0},{2,3},{3,2},{4,5},{5,4},{6,7},{7,6},{8,9},{9,8},{10,11... | collective-permute-start | bytes 3932168 | tf_op jit(solution)/shard_map/ppermute | solution.py:38
  701.9 42.9 %collective-permute-start.41 = (bf16[1280,768]{1,0:T(8,128)(2,1)}, bf16[1280,768]{1,0:T(8,128)(2,1)}, u32[]{:S(2)}, u32[]{:S(2)}) collective-permute-start(bf16[1280,768]{1,0:T(8,128)(2,1)} %get-tuple-element.100), channel_id=1, source_target_pairs={{0,4},{4,0},{8,12},{12,8},{16,20},{20,16},{24,28},{28,24},{1,5},{5... | collective-permute-start | bytes 5898248 | tf_op jit(solution)/shard_map/ppermute | solution.py:771
  701.9 32.0 %collective-permute-start.28 = (bf16[2,512,640]{2,1,0:T(8,128)(2,1)}, bf16[2,512,640]{2,1,0:T(8,128)(2,1)}, u32[]{:S(2)}, u32[]{:S(2)}) collective-permute-start(bf16[2,512,640]{2,1,0:T(8,128)(2,1)} %get-tuple-element.89), channel_id=1, source_target_pairs={{0,2},{1,3},{2,0},{3,1},{4,6},{5,7},{6,4},{7,5},{8,10},{9,11},{10,... | collective-permute-start | bytes 3932168 | tf_op jit(solution)/shard_map/ppermute | solution.py:38
  703.9 30.0 %copy-start.10 = (bf16[2,512,640]{2,1,0:T(8,128)(2,1)S(1)}, bf16[2,512,640]{2,1,0:T(8,128)(2,1)}, u32[]{:S(2)}) copy-start(bf16[2,512,640]{2,1,0:T(8,128)(2,1)} %copy-done.9) | copy-start | bytes 3932164
  703.9 3.8 collective-permute-start.36
  706.6 57.9 %collective-permute-start.32 = (bf16[2,512,640]{2,1,0:T(8,128)(2,1)}, bf16[2,512,640]{2,1,0:T(8,128)(2,1)}, u32[]{:S(2)}, u32[]{:S(2)}) collective-permute-start(bf16[2,512,640]{2,1,0:T(8,128)(2,1)} %get-tuple-element.95), channel_id=1, source_target_pairs={{0,2},{1,3},{2,0},{3,1},{4,6},{5,7},{6,4},{7,5},{8,10},{9,11},{10,... | collective-permute-start | bytes 3932168 | tf_op jit(solution)/shard_map/ppermute | solution.py:38
  707.8 4.2 collective-permute-start.37
  707.8 7.9 collective-permute-start.34
  712.0 55.4 %collective-permute-start.30 = (bf16[2,512,640]{2,1,0:T(8,128)(2,1)}, bf16[2,512,640]{2,1,0:T(8,128)(2,1)}, u32[]{:S(2)}, u32[]{:S(2)}) collective-permute-start(bf16[2,512,640]{2,1,0:T(8,128)(2,1)} %copy-done.28), channel_id=1, source_target_pairs={{0,1},{1,0},{2,3},{3,2},{4,5},{5,4},{6,7},{7,6},{8,9},{9,8},{10,11... | collective-permute-start | bytes 3932168 | tf_op jit(solution)/shard_map/ppermute | solution.py:38
  715.7 7.3 collective-permute-start.38
  723.1 38.6 %collective-permute-start.35 = (f32[4,256]{1,0:T(4,128)S(1)}, f32[4,256]{1,0:T(4,128)S(1)}, u32[]{:S(2)}, u32[]{:S(2)}) collective-permute-start(f32[4,256]{1,0:T(4,128)S(1)} %add.420), channel_id=1, source_target_pairs={{0,2},{1,3},{2,0},{3,1},{4,6},{5,7},{6,4},{7,5},{8,10},{9,11},{10,... | collective-permute-start | bytes 12296 | tf_op jit(solution)/shard_map/ppermute | solution.py:38
  733.9 9.4 %collective-permute-start.39 = (f32[8,320]{1,0:T(8,128)S(1)}, f32[8,320]{1,0:T(8,128)S(1)}, u32[]{:S(2)}, u32[]{:S(2)}) collective-permute-start(f32[8,320]{1,0:T(8,128)S(1)} %add.425), channel_id=1, source_target_pairs={{0,1},{1,0},{2,3},{3,2},{4,5},{5,4},{6,7},{7,6},{8,9},{9,8},{10,11... | collective-permute-start | bytes 30728 | tf_op jit(solution)/shard_map/ppermute | solution.py:38
  743.3 20.4 %collective-permute-start.40 = (f32[8,320]{1,0:T(8,128)S(1)}, f32[8,320]{1,0:T(8,128)S(1)}, u32[]{:S(2)}, u32[]{:S(2)}) collective-permute-start(f32[8,320]{1,0:T(8,128)S(1)} %add.426), channel_id=1, source_target_pairs={{0,2},{1,3},{2,0},{3,1},{4,6},{5,7},{6,4},{7,5},{8,10},{9,11},{10,... | collective-permute-start | bytes 30728 | tf_op jit(solution)/shard_map/ppermute | solution.py:38
  761.7 17.9 %collective-permute-start.27 = (bf16[512,640]{1,0:T(8,128)(2,1)}, bf16[512,640]{1,0:T(8,128)(2,1)}, u32[]{:S(2)}, u32[]{:S(2)}) collective-permute-start(bf16[512,640]{1,0:T(8,128)(2,1)} %fusion.38), channel_id=1, source_target_pairs={{0,2},{1,3},{2,0},{3,1},{4,6},{5,7},{6,4},{7,5},{8,10},{9,11},{10,... | collective-permute-start | bytes 1966088 | tf_op jit(solution)/shard_map/ppermute | solution.py:38
  763.1 18.1 %collective-permute-start.29 = (bf16[512,640]{1,0:T(8,128)(2,1)}, bf16[512,640]{1,0:T(8,128)(2,1)S(1)}, u32[]{:S(2)}, u32[]{:S(2)}) collective-permute-start(bf16[512,640]{1,0:T(8,128)(2,1)} %fusion.39), channel_id=1, source_target_pairs={{0,1},{1,0},{2,3},{3,2},{4,5},{5,4},{6,7},{7,6},{8,9},{9,8},{10,11... | collective-permute-start | bytes 1966088 | tf_op jit(solution)/shard_map/ppermute | solution.py:38
  765.9 27.3 %collective-permute-start.33 = (bf16[512,640]{1,0:T(8,128)(2,1)S(1)}, bf16[512,640]{1,0:T(8,128)(2,1)S(1)}, u32[]{:S(2)}, u32[]{:S(2)}) collective-permute-start(bf16[512,640]{1,0:T(8,128)(2,1)S(1)} %fusion.41), channel_id=1, source_target_pairs={{0,1},{1,0},{2,3},{3,2},{4,5},{5,4},{6,7},{7,6},{8,9},{9,8},{10,11... | collective-permute-start | bytes 1966088 | tf_op jit(solution)/shard_map/ppermute | solution.py:38
  768.7 26.1 %collective-permute-start.31 = (bf16[512,640]{1,0:T(8,128)(2,1)S(1)}, bf16[512,640]{1,0:T(8,128)(2,1)S(1)}, u32[]{:S(2)}, u32[]{:S(2)}) collective-permute-start(bf16[512,640]{1,0:T(8,128)(2,1)S(1)} %fusion.40), channel_id=1, source_target_pairs={{0,2},{1,3},{2,0},{3,1},{4,6},{5,7},{6,4},{7,5},{8,10},{9,11},{10,... | collective-permute-start | bytes 1966088 | tf_op jit(solution)/shard_map/ppermute | solution.py:38
  805.2 29.9 %copy-start.47 = (bf16[320,1920]{1,0:T(8,128)(2,1)S(1)}, bf16[320,1920]{1,0:T(8,128)(2,1)}, u32[]{:S(2)}) copy-start(bf16[320,1920]{1,0:T(8,128)(2,1)} %refs_0_.1) | copy-start | bytes 3686404
  838.5 41.4 %collective-permute-start.45 = (f32[320]{0:T(512)S(1)}, f32[320]{0:T(512)S(1)}, u32[]{:S(2)}, u32[]{:S(2)}) collective-permute-start(f32[320]{0:T(512)S(1)} %get-tuple-element.122), channel_id=1, source_target_pairs={{0,1},{1,0},{2,3},{3,2},{4,5},{5,4},{6,7},{7,6},{8,9},{9,8},{10,11... | collective-permute-start | bytes 3848 | tf_op jit(solution)/shard_map/ppermute | solution.py:38
  879.9 4.4 collective-permute-start.46
  (67 other events, 561.5 us)
Sparse Core Ops, SparseCore 0:
  82.9 124.8 all-gather.2
  209.5 140.6 all-gather.4
  538.7 33.2 reduce-scatter.6
  574.2 119.2 reduce-scatter.8
  695.6 137.3 reduce-scatter.10
  835.7 42.0 reduce-scatter.4

commit v11 on v10

--- a/solution.py
+++ b/solution.py
@@ -148,16 +148,15 @@
     return lax.all_to_all(block, "mdl", split_axis=1, concat_axis=0, tiled=True)
 
 
-def first_kernel(
-    parts, x_ref, w_ref, gain_ref, *refs
-):
+def first_kernel(parts, x_ref, w_ref, *refs):
     weights, (rows_ref, weight_ref), locals_ref = refs[:3], refs[3:5], refs[5:7]
     held, joined = refs[7:10], refs[10:12]
     own, x_sent, x_got, w_up, w_down, w_core, w_got = refs[12:]
     me, tok = lax.axis_index("mdl"), lax.axis_index("tok")
     pairs = lax.axis_size("tok") // 2
     level, last = tok // 2, pairs - 1
-    half, width, shard = x_ref.shape[0] // 2, x_ref.shape[1], w_ref.shape[0]
+    half, width = x_ref.shape[0] // 2, x_ref.shape[1]
+    shard, all_cols = w_ref.shape[0], weight_ref.shape[1]
     below, above = level > 0, level < last
 
     barrier = pltpu.get_barrier_semaphore()
@@ -178,79 +177,86 @@
     def cols(block):
         return pl.ds(pl.multiple_of(block * width, 128), width)
 
-    def block(index):
-        return weight_ref.at[pl.ds(pl.multiple_of(index * shard, 16), shard)]
+    piece = shard // 2
+
+    def block(index, part):
+        return weight_ref.at[pl.ds(pl.multiple_of(index * shard + part * piece, 16), piece)]
 
     def x_copy(source, target, at, to):
         return pltpu.make_async_remote_copy(
             source, target, x_sent.at[at], x_got.at[at], device_id={"mdl": me ^ to}
         )
 
-    def w_copy(source, index, sent, to):
+    def w_copy(source, index, part, sent, to):
         return pltpu.make_async_remote_copy(
-            source, block(index), sent, w_got.at[index], device_id={"tok": to}
+            source, block(index, part), sent, w_got.at[index, part], device_id={"tok": to}
         )
 
     mine = rows_ref.at[:, cols(me)]
     to_x, to_y = x_copy(x_ref, mine, 0, 1), x_copy(x_ref, mine, 1, 2)
-
-    @pl.when(above)
-    def _():
-        w_copy(w_ref, tok, w_up.at[0], tok + 2).start()
-
-    @pl.when(below)
-    def _():
-        w_copy(w_ref, tok, w_down.at[0], tok - 2).start()
-
-    to_x.start()
-    to_y.start()
-    w_copy(w_ref, tok, w_core.at[tok], tok ^ 1).start()
-    keep_x = pltpu.make_async_copy(x_ref, mine, own.at[0])
-    keep_w = pltpu.make_async_copy(w_ref, block(tok), own.at[1])
-    keep_x.start()
-    keep_w.start()
+    keeps = [pltpu.make_async_copy(x_ref, mine, own.at[0])]
+    for part in range(2):
+        source = w_ref.at[pl.ds(part * piece, piece), pl.ds(0, all_cols)]
+
+        @pl.when(above)
+        def _(source=source, part=part):
+            w_copy(source, tok, part, w_up.at[0, part], tok + 2).start()
+
+        @pl.when(below)
+        def _(source=source, part=part):
+            w_copy(source, tok, part, w_down.at[0, part], tok - 2).start()
+
+        w_copy(source, tok, part, w_core.at[tok, part], tok ^ 1).start()
+        keeps.append(pltpu.make_async_copy(source, block(tok, part), own.at[1 + part]))
+        if part == 0:
+            to_x.start()
+            to_y.start()
     loads = [
-        pltpu.make_async_copy(weight, to, own.at[2 + at])
+        pltpu.make_async_copy(weight, to, own.at[3 + at])
         for at, (weight, to) in enumerate(zip(weights, held))
     ]
-    for copy in loads:
+    for copy in (*keeps, *loads):
         copy.start()
     for copy in loads:
         copy.wait()
+    gain = w_ref[:, all_cols : all_cols + 1].astype(F32)
     for (start, stop), out in zip(parts, joined):
         count = stop - start
         for at, source in enumerate(held):
             value = source[:, start:stop]
             if at < 2:
-                value = (value.astype(F32) * gain_ref[...]).astype(BF16)
+                value = (value.astype(F32) * gain).astype(BF16)
             out[:, at * count : (at + 1) * count] = value
 
-    def relay(distance):
+    def relay(distance, part):
         low, high = tok - 2 * distance, tok + 2 * distance
 
         @pl.when(level >= distance)
         def _():
-            w_copy(block(low), low, w_core.at[low], tok ^ 1).wait_recv()
+            source = block(low, part)
+            w_copy(source, low, part, w_core.at[low, part], tok ^ 1).wait_recv()
 
             @pl.when(above)
             def _():
-                w_copy(block(low), low, w_up.at[distance], tok + 2).start()
-
-            w_copy(block(low), low, w_core.at[low], tok ^ 1).start()
+                w_copy(source, low, part, w_up.at[distance, part], tok + 2).start()
+
+            w_copy(source, low, part, w_core.at[low, part], tok ^ 1).start()
 
         @pl.when(level + distance <= last)
         def _():
-            w_copy(block(high), high, w_core.at[high], tok ^ 1).wait_recv()
+            source = block(high, part)
+            w_copy(source, high, part, w_core.at[high, part], tok ^ 1).wait_recv()
 
             @pl.when(below)
             def _():
-                w_copy(block(high), high, w_down.at[distance], tok - 2).start()
-
-            w_copy(block(high), high, w_core.at[high], tok ^ 1).start()
-
-    relay(1)
+                w_copy(source, high, part, w_down.at[distance, part], tok - 2).start()
+
+            w_copy(source, high, part, w_core.at[high, part], tok ^ 1).start()
+
+    relay(1, 0)
+    relay(1, 1)
     stores = [
-        pltpu.make_async_copy(out, to, own.at[5 + at])
+        pltpu.make_async_copy(out, to, own.at[6 + at])
         for at, (out, to) in enumerate(zip(joined, locals_ref))
     ]
     for copy in stores:
@@ -263,8 +269,9 @@
     to_y.wait_recv()
     bottom.start()
     for distance in range(2, pairs):
-        relay(distance)
-    for copy in (keep_x, keep_w, *stores):
+        relay(distance, 0)
+        relay(distance, 1)
+    for copy in (*keeps, *stores):
         copy.wait()
     for copy in (top, bottom):
         copy.wait_recv()
@@ -272,43 +279,45 @@
         copy.wait_send()
 
     for distance in range(pairs):
-
-        @pl.when((level >= distance) & above)
-        def _(distance=distance):
-            w_copy(block(tok), tok, w_up.at[distance], tok + 2).wait_send()
-
-        @pl.when((level + distance <= last) & below)
-        def _(distance=distance):
-            w_copy(block(tok), tok, w_down.at[distance], tok - 2).wait_send()
-
-        near, far = 2 * distance + tok % 2, 2 * distance + 1 - tok % 2
-        w_copy(block(near), near, w_core.at[near], tok ^ 1).wait_send()
-        w_copy(block(far), far, w_core.at[near], tok ^ 1).wait_recv()
-
-
-def first_gather(inputs, weight, gain, weights, parts):
+        for part in range(2):
+            mine = block(tok, part)
+
+            @pl.when((level >= distance) & above)
+            def _(mine=mine, distance=distance, part=part):
+                w_copy(mine, tok, part, w_up.at[distance, part], tok + 2).wait_send()
+
+            @pl.when((level + distance <= last) & below)
+            def _(mine=mine, distance=distance, part=part):
+                w_copy(mine, tok, part, w_down.at[distance, part], tok - 2).wait_send()
+
+            near, far = 2 * distance + tok % 2, 2 * distance + 1 - tok % 2
+            w_copy(block(near, part), near, part, w_core.at[near, part], tok ^ 1).wait_send()
+            w_copy(block(far, part), far, part, w_core.at[near, part], tok ^ 1).wait_recv()
+
+
+def first_gather(inputs, weight, weights, parts):
     tokens, width = inputs.shape
     shard, cols = weight.shape
     pairs = lax.axis_size("tok") // 2
     dma = pltpu.SemaphoreType.DMA
     locals_ff = [(shard, 3 * (stop - start)) for start, stop in parts]
-    shapes = [(tokens, 4 * width), (2 * pairs * shard, cols), *locals_ff]
+    shapes = [(tokens, 4 * width), (2 * pairs * shard, cols - 128), *locals_ff]
     *gathered, first, second = pl.pallas_call(
         functools.partial(first_kernel, parts),
         out_shape=[jax.ShapeDtypeStruct(shape, BF16) for shape in shapes],
-        in_specs=[pl.BlockSpec(memory_space=pltpu.VMEM)] * 3
+        in_specs=[pl.BlockSpec(memory_space=pltpu.VMEM)] * 2
         + [pl.BlockSpec(memory_space=pl.ANY)] * 3,
         out_specs=[pl.BlockSpec(memory_space=pl.ANY)] * 4,
         scratch_shapes=[pltpu.VMEM(array.shape, BF16) for array in weights]
         + [pltpu.VMEM(shape, BF16) for shape in locals_ff]
         + [
-            dma((7,)), dma((4,)), dma((4,)), dma((pairs,)), dma((pairs,)),
-            dma((2 * pairs,)), dma((2 * pairs,)),
+            dma((8,)), dma((4,)), dma((4,)), dma((pairs, 2)), dma((pairs, 2)),
+            dma((2 * pairs, 2)), dma((2 * pairs, 2)),
         ],
         compiler_params=pltpu.CompilerParams(
             collective_id=0, has_side_effects=True, vmem_limit_bytes=60 << 20
         ),
-    )(inputs, weight, gain, *weights)
+    )(inputs, weight, *weights)
     return *gathered, (first, second)
 
 
@@ -781,10 +790,10 @@
     middle = ff_cols // 256 * 128
     parts = ((0, middle), (middle, ff_cols))
     if size == 4 and lax.axis_size("tok") == 8:
+        gain_cols = jnp.broadcast_to(norm2_gain[:, None], (norm2_gain.shape[0], 128))
         rows_in, w_attn, locals_ff = first_gather(
             inputs,
-            attn_local,
-            norm2_gain.astype(F32)[:, None],
+            jnp.concatenate([attn_local, gain_cols], axis=1),
             (gate_weight, up_weight, down_weight.T),
             parts,
         )

time: 900 us -> 898 us (level)
  no operation moved by 1% of the time
where the time goes in v11:
time: 898 us; the launch traced here: 890 us
  waiting for transfers between devices  342 us (38%)
  Pallas kernels  264 us (29%)
  other arithmetic  71.4 us (8%)
  matrix products  68.5 us (8%)
  starting transfers between devices  58.9 us (7%)
  local copies, waits for them, and re-layouts  50.6 us (6%)
  blocking collectives  18.5 us (2%)
  between operations  15.3 us (2%)
    ppermute x40, waiting for transfers between devices, swap(): return lax.ppermute(block, 'mdl', [(i, i ^ distance) for i in range(size)])  204 us
    dot_general x7, matrix products, nn(): return jnp.dot(left_op, right_op, preferred_element_type=F32)  68.5 us
    pallas_call x1, Pallas kernels, first_gather(): pl.pallas_call(functools.partial(first_kernel, parts), out_shape=[jax.Sha...  67 us
    reduce_scatter x4, waiting for transfers between devices, pair_to_tok(): lax.psum_scatter(both, 'tok', scatter_dimension=0, tiled=True, axis_index...  65.6 us
    pallas_call x4, Pallas kernels, scatter_product(): pl.pallas_call(functools.partial(payload_kernel, starts), grid_spec=pltpu...  50 us
    pallas_call x2, Pallas kernels, part_grad(): pl.pallas_call(part_kernel, grid=(pairs,), out_shape=(out, out), in_specs...  48.5 us
    ppermute x40, starting transfers between devices, swap(): return lax.ppermute(block, 'mdl', [(i, i ^ distance) for i in range(size)])  45.3 us
    all_to_all x2, waiting for transfers between devices, rows_to_cols(): return lax.all_to_all(block, 'mdl', split_axis=0, concat_axis=1, tiled=True)  35.3 us
  transfers between devices with their start and end apart: 56, of which 30 were waited for; matrix products, arithmetic and copies ran while one was open for 13% of the time, Pallas kernels for 20%

profile of v11, /device:TPU:0, one launch (start us, length us, event | category | flops | bytes accessed | tf_op | source)
XLA Modules:
  0.0 889.7 jit_solution(1376947494389327232)
XLA Ops:
  11.9 67.0 %shard_map.169 = (bf16[1024,2560]{1,0:T(8,128)(2,1)}, bf16[2560,1408]{1,0:T(8,128)(2,1)}, bf16[320,2688]{1,0:T(8,128)(2,1)}, bf16[320,3072]{1,0:T(8,128)(2,1)}) custom-call(bf16[1024,640]{1,0:T(8,128)(2,1)} %x_ref.1, bf16[320,1536]{1,0:T(8,128)(2,1)} %pad_maximum_fusion.3.w_ref, bf16[320,1920]{1,0:T(8,128)(2,1)} %refs_0_.1, bf16[320,1920]{1,0:T(8,128)(2,1)} %refs_1_.1, ...), custom_call_target="tpu_custom_call" | custom-call | tf_op jit(solution)/shard_map/pallas_call | solution.py:305
  79.7 9.0 %fusion.30 = bf16[1024,768]{1,0:T(8,128)(2,1)} fusion(bf16[1024,2560]{1,0:T(8,128)(2,1)} %get-tuple-element.91.left_ref, bf16[2560,1408]{1,0:T(8,128)(2,1)} %get-tuple-element.60.refs_1_.refs_5_.refs_0_), kind=kOutput, calls=%fused_computation.57 | convolution fusion | flops 4027318272 | bytes 10747904 | tf_op jit(solution)/shard_map/dot_general | solution.py:33
  88.7 3.8 all-to-all-start
  94.3 18.2 %all-to-all-done = bf16[4,256,768]{2,1,0:T(8,128)(2,1)S(1)} async-done(((bf16[4,256,768]{2,1,0:T(8,128)(2,1)}), bf16[4,256,768]{2,1,0:T(8,128)(2,1)S(1)}, u32[]{:S(2)}, u32[]{:S(2)}) %all-to-all-start) | async-done | bytes 1572896 | tf_op jit(solution)/shard_map/all_to_all | solution.py:144
  117.5 5.6 collective-permute-done
  130.6 11.2 %att_f.1 = (bf16[256,2560]{1,0:T(8,128)(2,1)S(1)}, f32[10,256,1]{2,1,0:T(8,128)S(1)}) custom-call(s32[1]{0:T(128)} %bitcast.1.first_ref, bf16[256,3072]{1,0:T(8,128)(2,1)S(1)} %bitcast.129, bf16[1024,512]{1,0:T(8,128)(2,1)S(1)} %constant_dynamic-update-slice_fusion.4.kv_ref, f32[256,128]{1,0:T(8,128)S(1)} %get-tuple-element.145.cos_ref, ...), custom_call_target="tpu_custom_call" | custom-call | flops 2684354560 | bytes 3670016 | tf_op jit(solution)/shard_map/att_f/pallas_call | solution.py:402
  142.0 18.5 %all_to_all.76 = bf16[256,4,640]{2,0,1:T(8,128)(2,1)} all-to-all(bf16[256,4,640]{2,0,1:T(8,128)(2,1)S(1)} %bitcast.138), channel_id=1, replica_groups=mesh['tok'=8,'mdl'=4] {'mdl'}, dimensions={1} | all-to-all | bytes 2621440 | tf_op jit(solution)/shard_map/all_to_all | solution.py:148
  160.5 7.9 shard_map.170
  169.9 25.7 %collective-permute-done.4 = bf16[2,512,640]{2,1,0:T(8,128)(2,1)S(1)} collective-permute-done((bf16[2,512,640]{2,1,0:T(8,128)(2,1)S(1)}, bf16[2,512,640]{2,1,0:T(8,128)(2,1)S(1)}, u32[]{:S(2)}, u32[]{:S(2)}) %collective-permute-start.4) | collective-permute-done | bytes 1310752 | tf_op jit(solution)/shard_map/ppermute | solution.py:38
  200.6 10.1 %collective-permute-done.5 = bf16[512,640]{1,0:T(8,128)(2,1)S(1)} collective-permute-done((bf16[512,640]{1,0:T(8,128)(2,1)}, bf16[512,640]{1,0:T(8,128)(2,1)S(1)}, u32[]{:S(2)}, u32[]{:S(2)}) %collective-permute-start.5) | collective-permute-done | bytes 655392 | tf_op jit(solution)/shard_map/ppermute | solution.py:38
  214.4 3.5 broadcast_in_dim.13
  221.3 24.4 %collective-permute-done.8 = bf16[1024,640]{1,0:T(8,128)(2,1)S(1)} collective-permute-done((bf16[1024,640]{1,0:T(8,128)(2,1)S(1)}, bf16[1024,640]{1,0:T(8,128)(2,1)S(1)}, u32[]{:S(2)}, u32[]{:S(2)}) %collective-permute-start.8) | collective-permute-done | bytes 1310752 | tf_op jit(solution)/shard_map/ppermute | solution.py:38
  255.0 4.8 collective-permute-done.10
  262.8 3.6 fusion
  266.5 5.8 fusion.1.rows_ref
  272.2 9.7 %fusion.12 = f32[896,1024]{0,1:T(8,128)S(1)} fusion(bf16[1024,2560]{1,0:T(8,128)(2,1)} %above_ref.2, bf16[2560,2688]{1,0:T(8,128)(2,1)} %all-gather.3.cloned.1.call-done.refs_2_.refs_1_), kind=kOutput, calls=%fused_computation.15 | convolution fusion | flops 4697620480 | bytes 13500416 | tf_op jit(solution)/shard_map/dot_general | solution.py:33
  281.9 7.9 fusion.8
  289.8 9.3 %add_reduce_fusion.1 = (f32[1024]{0:T(1024)S(1)}, bf16[1024,896]{1,0:T(8,128)(2,1)S(1)}, bf16[1024,896]{1,0:T(8,128)(2,1)S(1)}, bf16[1024,896]{1,0:T(8,128)(2,1)S(1)}) fusion(f32[1024,896]{1,0:T(8,128)S(1)} %fusion.8, f32[896,1024]{0,1:T(8,128)S(1)} %fusion.12, bf16[1024,2560]{1,0:T(8,128)(2,1)S(1)} %copy-done.46, ...), kind=kOutput, calls=%fused_computation.29 | convolution fusion | flops 4723309568 | bytes 22679552 | tf_op jit(solution)/shard_map/dot_general | solution.py:33
  299.1 23.6 %shard_map.171 = (bf16[1280,2688]{1,0:T(8,128)(2,1)}, bf16[1280,2688]{1,0:T(8,128)(2,1)}) custom-call(s32[1]{0:T(128)} %bitcast.14.core_ref, bf16[1024,2560]{1,0:T(8,128)(2,1)} %fusion.1.rows_ref, bf16[1024,2560]{1,0:T(8,128)(2,1)} %above_ref.2, bf16[1024,896]{1,0:T(8,128)(2,1)S(1)} %get-tuple-element.71.d_gate_ref.refs_0_, ...), custom_call_target="tpu_custom_call" | custom-call | flops 14092861440 | bytes 29753344 | tf_op jit(solution)/shard_map/pallas_call | solution.py:542
  322.7 15.3 %shard_map.172.refs_3_ = f32[1024,2560]{1,0:T(8,128)} custom-call(bf16[1024,896]{1,0:T(8,128)(2,1)S(1)} %get-tuple-element.71.d_gate_ref.refs_0_, bf16[1024,896]{1,0:T(8,128)(2,1)S(1)} %get-tuple-element.119.d_up_ref.refs_1_, bf16[2560,2688]{1,0:T(8,128)(2,1)} %all-gather.3.cloned.1.call-done.refs_2_.refs_1_), custom_call_target="tpu_custom_call" | custom-call | flops 9395240960 | bytes 24248320 | tf_op jit(solution)/shard_map/pallas_call | solution.py:643
  338.0 10.0 %all-gather.5.cloned.1.call-done.refs_2_.refs_1_ = bf16[2560,3072]{1,0:T(8,128)(2,1)} async-done(((bf16[320,3072]{1,0:T(8,128)(2,1)}), bf16[2560,3072]{1,0:T(8,128)(2,1)}) %all-gather.5.cloned.1.call-update) | async-done | bytes 15728656 | tf_op jit(solution)/shard_map/all_gather | solution.py:775
  348.0 10.7 %fusion.2 = f32[1024,1024]{1,0:T(8,128)} fusion(bf16[1024,2560]{1,0:T(8,128)(2,1)} %above_ref.2, bf16[2560,3072]{1,0:T(8,128)(2,1)} %all-gather.5.cloned.1.call-done.refs_2_.refs_1_), kind=kOutput, calls=%fused_computation.5 | convolution fusion | flops 5368709120 | bytes 14680064 | tf_op jit(solution)/shard_map/dot_general | solution.py:33
  358.7 8.9 %fusion.4 = f32[1024,1024]{1,0:T(8,128)} fusion(bf16[1024,2560]{1,0:T(8,128)(2,1)} %fusion.1.rows_ref, bf16[2560,3072]{1,0:T(8,128)(2,1)S(1)} %copy-done.42), kind=kOutput, calls=%fused_computation.7 | convolution fusion | flops 5368709120 | bytes 14680064 | tf_op jit(solution)/shard_map/dot_general | solution.py:33
  367.6 13.0 %fusion.67 = (bf16[1024,1024]{1,0:T(8,128)(2,1)}, f32[1024]{0:T(1024)S(1)}, bf16[1024,1024]{1,0:T(8,128)(2,1)}, bf16[1024,1024]{1,0:T(8,128)(2,1)}) fusion(f32[1024,1024]{1,0:T(8,128)} %fusion.2, f32[1024,1024]{1,0:T(8,128)} %fusion.4, bf16[1024,2560]{1,0:T(8,128)(2,1)S(1)} %bitcast.137, bf16[2560,3072]{1,0:T(8,128)(2,1)S(1)} %copy-done.42), kind=kOutput, calls=%fused_computation.158 | convolution fusion | flops 5398068224 | bytes 25169920 | tf_op jit(solution)/shard_map/dot_general | solution.py:33
  380.6 18.7 %shard_map.173 = (bf16[2,512,640]{2,1,0:T(8,128)(2,1)S(1)}, bf16[2,512,640]{2,1,0:T(8,128)(2,1)S(1)}, bf16[2,512,640]{2,1,0:T(8,128)(2,1)S(1)}, bf16[2,512,640]{2,1,0:T(8,128)(2,1)S(1)}) custom-call(s32[1]{0:T(128)} %bitcast.me_ref, bf16[1024,1024]{1,0:T(8,128)(2,1)} %get-tuple-element.113.refs_0_.d_gate_ref, ...), custom_call_target="tpu_custom_call" | custom-call | flops 10737418240 | bytes 25165824 | tf_op jit(solution)/shard_map/pallas_call | solution.py:684
  402.9 28.7 %collective-permute-done.16 = f32[8,128]{1,0:T(8,128)S(1)} collective-permute-done((f32[8,128]{1,0:T(8,128)S(1)}, f32[8,128]{1,0:T(8,128)S(1)}, u32[]{:S(2)}, u32[]{:S(2)}) %collective-permute-start.16) | collective-permute-done | bytes 4128 | tf_op jit(solution)/shard_map/ppermute | solution.py:38
  436.5 24.9 %shard_map.174 = (bf16[1280,3072]{1,0:T(8,128)(2,1)}, bf16[1280,3072]{1,0:T(8,128)(2,1)}) custom-call(s32[1]{0:T(128)} %bitcast.14.core_ref, bf16[1024,2560]{1,0:T(8,128)(2,1)} %fusion.1.rows_ref, bf16[1024,2560]{1,0:T(8,128)(2,1)} %above_ref.2, bf16[1024,1024]{1,0:T(8,128)(2,1)S(1)} %copy-done.31, bf16[1024,1024]{1,0:T(8,128)(2,1)S(1)} %copy-done.32, ...), custom_call_target="tpu_custom_call" | custom-call | flops 16106127360 | bytes 32505856 | tf_op jit(solution)/shard_map/pallas_call | solution.py:542
  464.4 3.9 fusion.70
  469.7 27.6 %collective-permute-done.20.refs_2_ = bf16[1024,640]{1,0:T(8,128)(2,1)S(1)} collective-permute-done((bf16[1024,640]{1,0:T(8,128)(2,1)S(1)}, bf16[1024,640]{1,0:T(8,128)(2,1)S(1)}, u32[]{:S(2)}, u32[]{:S(2)}) %collective-permute-start.20) | collective-permute-done | bytes 1310752 | tf_op jit(solution)/shard_map/ppermute | solution.py:38
  500.2 11.4 %collective-permute-done.22.refs_4_ = bf16[512,640]{1,0:T(8,128)(2,1)S(1)} collective-permute-done((bf16[512,640]{1,0:T(8,128)(2,1)S(1)}, bf16[512,640]{1,0:T(8,128)(2,1)S(1)}, u32[]{:S(2)}, u32[]{:S(2)}) %collective-permute-start.22) | collective-permute-done | bytes 655392 | tf_op jit(solution)/shard_map/ppermute | solution.py:38
  512.6 6.9 shard_map.177
  519.6 8.0 shard_map.181
  527.6 3.7 collective-permute-done.42.right_ref
  532.7 3.6 shard_map.182
  536.4 3.0 copy-done.3
  539.4 6.8 shard_map.183
  549.3 12.5 %collective-permute-done.44.right_ref = bf16[1280,3072]{1,0:T(8,128)(2,1)S(1)} collective-permute-done((bf16[1280,3072]{1,0:T(8,128)(2,1)}, bf16[1280,3072]{1,0:T(8,128)(2,1)S(1)}, u32[]{:S(2)}, u32[]{:S(2)}) %collective-permute-start.44) | collective-permute-done | bytes 7864352 | tf_op jit(solution)/shard_map/ppermute | solution.py:780
  561.8 3.3 copy-done.2
  567.0 3.1 copy-done
  570.1 4.8 all-to-all-start.2
  574.9 17.1 %all-to-all-done.2 = bf16[4,256,640]{2,1,0:T(8,128)(2,1)} async-done(((bf16[4,256,640]{2,1,0:T(8,128)(2,1)}), bf16[4,256,640]{2,1,0:T(8,128)(2,1)}, u32[]{:S(2)}, u32[]{:S(2)}) %all-to-all-start.2) | async-done | bytes 1310752 | tf_op jit(solution)/shard_map/all_to_all | solution.py:144
  596.3 15.6 %att_b.1 = (bf16[256,2560]{1,0:T(8,128)(2,1)S(1)}, f32[1024,512]{1,0:T(8,128)S(1)}) custom-call(s32[1]{0:T(128)} %bitcast.1.first_ref, bf16[256,3072]{1,0:T(8,128)(2,1)S(1)} %bitcast.130, bf16[1024,512]{1,0:T(8,128)(2,1)S(1)} %copy-done.19, f32[256,128]{1,0:T(8,128)S(1)} %copy-done.27, f32[256,128]{1,0:T(8,128)S(1)} %copy-done.25, s32[256,1]{1,0:T(8,128)S(1)} %copy-done.21, ...), custom_call_target="tpu_custom_call" | custom-call | flops 6710886400 | bytes 8388608 | tf_op jit(solution)/shard_map/att_b/pallas_call | solution.py:428
  615.0 4.8 collective-permute-done.23
  622.0 3.7 collective-permute-done.24
  628.9 3.8 collective-permute-done.26
  637.0 4.3 all-to-all-start.3
  641.4 3.7 multiply_reduce_fusion
  645.1 13.5 %shard_map.175.refs_2_ = f32[1024,2560]{1,0:T(8,128)} custom-call(bf16[1024,896]{1,0:T(8,128)(2,1)S(1)} %get-tuple-element.81.hidden_ref.refs_0_, bf16[2560,2688]{1,0:T(8,128)(2,1)} %all-gather.3.cloned.1.call-done.refs_2_.refs_1_), custom_call_target="tpu_custom_call" | custom-call | flops 4697620480 | bytes 24248320 | tf_op jit(solution)/shard_map/pallas_call | solution.py:643
  658.6 14.1 %shard_map.176 = (bf16[2,512,640]{2,1,0:T(8,128)(2,1)}, bf16[2,512,640]{2,1,0:T(8,128)(2,1)}, bf16[2,512,640]{2,1,0:T(8,128)(2,1)S(1)}, bf16[2,512,640]{2,1,0:T(8,128)(2,1)S(1)}) custom-call(s32[1]{0:T(128)} %bitcast.me_ref, bf16[1024,1024]{1,0:T(8,128)(2,1)} %get-tuple-element.80.hidden_ref.refs_0_, ...), custom_call_target="tpu_custom_call" | custom-call | flops 5368709120 | bytes 23068672 | tf_op jit(solution)/shard_map/pallas_call | solution.py:684
  676.8 9.3 %shard_map.178 = (bf16[2,512,640]{2,1,0:T(8,128)(2,1)S(1)}, bf16[2,512,640]{2,1,0:T(8,128)(2,1)}, bf16[2,512,640]{2,1,0:T(8,128)(2,1)S(1)}, bf16[2,512,640]{2,1,0:T(8,128)(2,1)S(1)}) custom-call(s32[1]{0:T(128)} %bitcast.me_ref, bf16[1024,768]{1,0:T(8,128)(2,1)} %bitcast.35.refs_0_, bf16[2560,1408]{1,0:T(8,128)(2,1)} %get-tuple-element.60.refs_1_.refs_5_.refs_0_), custom_call_target="tpu_custom_call" | custom-call | flops 4026531840 | bytes 14024704 | tf_op jit(solution)/shard_map/pallas_call | solution.py:684
  690.5 9.2 %shard_map.179 = (bf16[1280,768]{1,0:T(8,128)(2,1)S(1)}, bf16[1280,768]{1,0:T(8,128)(2,1)}, f32[2560,1]{1,0:T(8,128)S(1)}) custom-call(s32[1]{0:T(128)} %bitcast.14.core_ref, bf16[1024,2560]{1,0:T(8,128)(2,1)} %get-tuple-element.91.left_ref, bf16[1024,768]{1,0:T(8,128)(2,1)S(1)} %multiply_convert_fusion.2.right_ref, ...), custom_call_target="tpu_custom_call" | custom-call | flops 4026531840 | bytes 10747904 | tf_op jit(solution)/shard_map/pallas_call | solution.py:509
  706.7 3.1 collective-permute-done.37
  713.6 7.2 collective-permute-done.38
  722.3 9.4 %collective-permute-done.28 = bf16[2,512,640]{2,1,0:T(8,128)(2,1)} collective-permute-done((bf16[2,512,640]{2,1,0:T(8,128)(2,1)}, bf16[2,512,640]{2,1,0:T(8,128)(2,1)}, u32[]{:S(2)}, u32[]{:S(2)}) %collective-permute-start.28) | collective-permute-done | bytes 1310752 | tf_op jit(solution)/shard_map/ppermute | solution.py:38
  733.8 7.3 collective-permute-done.39
  742.6 6.8 shard_map.180
  749.5 10.0 %collective-permute-done.35 = f32[4,256]{1,0:T(4,128)S(1)} collective-permute-done((f32[4,256]{1,0:T(4,128)S(1)}, f32[4,256]{1,0:T(4,128)S(1)}, u32[]{:S(2)}, u32[]{:S(2)}) %collective-permute-start.35) | collective-permute-done | bytes 4128 | tf_op jit(solution)/shard_map/ppermute | solution.py:38
  767.1 10.3 %collective-permute-done.27 = bf16[512,640]{1,0:T(8,128)(2,1)} collective-permute-done((bf16[512,640]{1,0:T(8,128)(2,1)}, bf16[512,640]{1,0:T(8,128)(2,1)}, u32[]{:S(2)}, u32[]{:S(2)}) %collective-permute-start.27) | collective-permute-done | bytes 655392 | tf_op jit(solution)/shard_map/ppermute | solution.py:38
  780.4 10.6 %collective-permute-done.33 = bf16[512,640]{1,0:T(8,128)(2,1)S(1)} collective-permute-done((bf16[512,640]{1,0:T(8,128)(2,1)S(1)}, bf16[512,640]{1,0:T(8,128)(2,1)S(1)}, u32[]{:S(2)}, u32[]{:S(2)}) %collective-permute-start.33) | collective-permute-done | bytes 655392 | tf_op jit(solution)/shard_map/ppermute | solution.py:38
  794.6 3.2 fusion.22
  799.7 3.2 fusion.74
  803.0 27.8 %reduce-scatter.11.cloned.1.call-done = bf16[320,3072]{1,0:T(8,128)(2,1)} async-done(((bf16[1280,3072]{1,0:T(8,128)(2,1)}), bf16[320,3072]{1,0:T(8,128)(2,1)}) %reduce-scatter.11.cloned.1.call-update) | async-done | bytes 1966096 | tf_op jit(solution)/shard_map/reduce_scatter | solution.py:783
  833.3 2.9 fusion.26
  837.7 37.8 %reduce-scatter.5.cloned.1.call-done = bf16[320,768]{1,0:T(8,128)(2,1)} async-done(((bf16[1280,768]{1,0:T(8,128)(2,1)}), bf16[320,768]{1,0:T(8,128)(2,1)}) %reduce-scatter.5.cloned.1.call-update) | async-done | bytes 491536 | tf_op jit(solution)/shard_map/reduce_scatter | solution.py:783
  (331 shorter events, 137.2 us)
Async XLA Ops:
  7.2 265.1 %all-gather.3.cloned.1.call-start = ((), (), s32[]{:S(2)}) async-start(), calls=%async_computation.8 | async-start | bytes 15482880 | tf_op jit(solution)/shard_map/all_gather | solution.py:775
  78.9 269.0 %all-gather.5.cloned.1.call-start = ((), (), s32[]{:S(2)}) async-start(), calls=%async_computation.9 | async-start | bytes 17694720 | tf_op jit(solution)/shard_map/all_gather | solution.py:775
  88.7 23.8 %all-to-all-start = ((bf16[4,256,768]{2,1,0:T(8,128)(2,1)}), bf16[4,256,768]{2,1,0:T(8,128)(2,1)S(1)}, u32[]{:S(2)}, u32[]{:S(2)}) async-start(bf16[4,256,768]{2,1,0:T(8,128)(2,1)} %bitcast.4), calls=%async_computation | async-start | bytes 3145728 | tf_op jit(solution)/shard_map/all_to_all | solution.py:144
  92.6 705.2 %reduce-scatter.7.cloned.1.call-start = ((), (), s32[]{:S(2)}) async-start(), calls=%async_computation.11 | async-start | bytes 2048000 | tf_op jit(solution)/shard_map/reduce_scatter | solution.py:783
  114.3 27.5 %copy-start.24 = (f32[256,128]{1,0:T(8,128)}, f32[256,128]{1,0:T(8,128)S(1)}, u32[]{:S(2)}) copy-start(f32[256,128]{1,0:T(8,128)S(1)} %get-tuple-element.144.sin_ref) | copy-start | bytes 393220
  115.2 7.9 collective-permute-start
  116.6 8.0 collective-permute-start.1
  123.1 5.0 collective-permute-start.2
  125.5 5.0 collective-permute-start.3
  168.4 27.2 %collective-permute-start.4 = (bf16[2,512,640]{2,1,0:T(8,128)(2,1)S(1)}, bf16[2,512,640]{2,1,0:T(8,128)(2,1)S(1)}, u32[]{:S(2)}, u32[]{:S(2)}) collective-permute-start(bf16[2,512,640]{2,1,0:T(8,128)(2,1)S(1)} %get-tuple-element.63), channel_id=1, source_target_pairs={{0,1},{1,0},{2,3},{3,2},{4,5},{5,4},{6,7},{7,6},{8,9},{9,8},{10,11... | collective-permute-start | bytes 3932168 | tf_op jit(solution)/shard_map/ppermute | solution.py:38
  169.4 28.7 %collective-permute-start.6 = (bf16[2,512,640]{2,1,0:T(8,128)(2,1)S(1)}, bf16[2,512,640]{2,1,0:T(8,128)(2,1)S(1)}, u32[]{:S(2)}, u32[]{:S(2)}) collective-permute-start(bf16[2,512,640]{2,1,0:T(8,128)(2,1)S(1)} %get-tuple-element.65), channel_id=1, source_target_pairs={{0,2},{1,3},{2,0},{3,1},{4,6},{5,7},{6,4},{7,5},{8,10},{9,11},{10,... | collective-permute-start | bytes 3932168 | tf_op jit(solution)/shard_map/ppermute | solution.py:38
  196.8 13.9 %collective-permute-start.5 = (bf16[512,640]{1,0:T(8,128)(2,1)}, bf16[512,640]{1,0:T(8,128)(2,1)S(1)}, u32[]{:S(2)}, u32[]{:S(2)}) collective-permute-start(bf16[512,640]{1,0:T(8,128)(2,1)} %fusion.34), channel_id=1, source_target_pairs={{0,2},{1,3},{2,0},{3,1},{4,6},{5,7},{6,4},{7,5},{8,10},{9,11},{10,... | collective-permute-start | bytes 1966088 | tf_op jit(solution)/shard_map/ppermute | solution.py:38
  200.1 12.8 %collective-permute-start.7 = (bf16[512,640]{1,0:T(8,128)(2,1)}, bf16[512,640]{1,0:T(8,128)(2,1)}, u32[]{:S(2)}, u32[]{:S(2)}) collective-permute-start(bf16[512,640]{1,0:T(8,128)(2,1)} %fusion.35), channel_id=1, source_target_pairs={{0,1},{1,0},{2,3},{3,2},{4,5},{5,4},{6,7},{7,6},{8,9},{9,8},{10,11... | collective-permute-start | bytes 1966088 | tf_op jit(solution)/shard_map/ppermute | solution.py:38
  219.7 26.0 %collective-permute-start.8 = (bf16[1024,640]{1,0:T(8,128)(2,1)S(1)}, bf16[1024,640]{1,0:T(8,128)(2,1)S(1)}, u32[]{:S(2)}, u32[]{:S(2)}) collective-permute-start(bf16[1024,640]{1,0:T(8,128)(2,1)S(1)} %get-tuple-element.112), channel_id=1, source_target_pairs={{0,1},{1,0},{2,3},{3,2},{4,5},{5,4},{6,7},{7,6},{8,9},{9,8},{10,11... | collective-permute-start | bytes 3932168 | tf_op jit(solution)/shard_map/ppermute | solution.py:38
  219.8 27.9 %collective-permute-start.9 = (bf16[1024,640]{1,0:T(8,128)(2,1)S(1)}, bf16[1024,640]{1,0:T(8,128)(2,1)S(1)}, u32[]{:S(2)}, u32[]{:S(2)}) collective-permute-start(bf16[1024,640]{1,0:T(8,128)(2,1)S(1)} %get-tuple-element.112), channel_id=1, source_target_pairs={{0,2},{1,3},{2,0},{3,1},{4,6},{5,7},{6,4},{7,5},{8,10},{9,11},{10,... | collective-permute-start | bytes 3932168 | tf_op jit(solution)/shard_map/ppermute | solution.py:38
  246.6 13.2 %collective-permute-start.10 = (bf16[512,640]{1,0:T(8,128)(2,1)}, bf16[512,640]{1,0:T(8,128)(2,1)S(1)}, u32[]{:S(2)}, u32[]{:S(2)}) collective-permute-start(bf16[512,640]{1,0:T(8,128)(2,1)} %slice.270), channel_id=1, source_target_pairs={{0,2},{1,3},{2,0},{3,1},{4,6},{5,7},{6,4},{7,5},{8,10},{9,11},{10,... | collective-permute-start | bytes 1966088 | tf_op jit(solution)/shard_map/ppermute | solution.py:38
  249.6 11.2 %collective-permute-start.11 = (bf16[512,640]{1,0:T(8,128)(2,1)}, bf16[512,640]{1,0:T(8,128)(2,1)}, u32[]{:S(2)}, u32[]{:S(2)}) collective-permute-start(bf16[512,640]{1,0:T(8,128)(2,1)} %slice.271), channel_id=1, source_target_pairs={{0,1},{1,0},{2,3},{3,2},{4,5},{5,4},{6,7},{7,6},{8,9},{9,8},{10,11... | collective-permute-start | bytes 1966088 | tf_op jit(solution)/shard_map/ppermute | solution.py:38
  380.6 55.9 %copy-start.32 = (bf16[1024,1024]{1,0:T(8,128)(2,1)S(1)}, bf16[1024,1024]{1,0:T(8,128)(2,1)}, u32[]{:S(2)}) copy-start(bf16[1024,1024]{1,0:T(8,128)(2,1)} %get-tuple-element.117.refs_1_.d_up_ref) | copy-start | bytes 6291460
  399.4 37.2 %copy-start.31 = (bf16[1024,1024]{1,0:T(8,128)(2,1)S(1)}, bf16[1024,1024]{1,0:T(8,128)(2,1)}, u32[]{:S(2)}) copy-start(bf16[1024,1024]{1,0:T(8,128)(2,1)} %get-tuple-element.113.refs_0_.d_gate_ref) | copy-start | bytes 6291460
  399.4 32.8 %collective-permute-start.14 = (bf16[2,512,640]{2,1,0:T(8,128)(2,1)S(1)}, bf16[2,512,640]{2,1,0:T(8,128)(2,1)S(1)}, u32[]{:S(2)}, u32[]{:S(2)}) collective-permute-start(bf16[2,512,640]{2,1,0:T(8,128)(2,1)S(1)} %get-tuple-element.75), channel_id=1, source_target_pairs={{0,2},{1,3},{2,0},{3,1},{4,6},{5,7},{6,4},{7,5},{8,10},{9,11},{10,... | collective-permute-start | bytes 3932168 | tf_op jit(solution)/shard_map/ppermute | solution.py:38
  400.9 33.0 %collective-permute-start.12 = (bf16[2,512,640]{2,1,0:T(8,128)(2,1)S(1)}, bf16[2,512,640]{2,1,0:T(8,128)(2,1)S(1)}, u32[]{:S(2)}, u32[]{:S(2)}) collective-permute-start(bf16[2,512,640]{2,1,0:T(8,128)(2,1)S(1)} %get-tuple-element.73), channel_id=1, source_target_pairs={{0,1},{1,0},{2,3},{3,2},{4,5},{5,4},{6,7},{7,6},{8,9},{9,8},{10,11... | collective-permute-start | bytes 3932168 | tf_op jit(solution)/shard_map/ppermute | solution.py:38
  402.4 29.3 %collective-permute-start.16 = (f32[8,128]{1,0:T(8,128)S(1)}, f32[8,128]{1,0:T(8,128)S(1)}, u32[]{:S(2)}, u32[]{:S(2)}) collective-permute-start(f32[8,128]{1,0:T(8,128)S(1)} %add_bitcast_fusion), channel_id=1, source_target_pairs={{0,1},{1,0},{2,3},{3,2},{4,5},{5,4},{6,7},{7,6},{8,9},{9,8},{10,11... | collective-permute-start | bytes 12296 | tf_op jit(solution)/shard_map/ppermute | solution.py:38
  431.6 29.8 %collective-permute-start.17 = (f32[8,128]{1,0:T(8,128)S(1)}, f32[8,128]{1,0:T(8,128)S(1)}, u32[]{:S(2)}, u32[]{:S(2)}) collective-permute-start(f32[8,128]{1,0:T(8,128)S(1)} %fusion.82), channel_id=1, source_target_pairs={{0,2},{1,3},{2,0},{3,1},{4,6},{5,7},{6,4},{7,5},{8,10},{9,11},{10,... | collective-permute-start | bytes 12296 | tf_op jit(solution)/shard_map/ppermute | solution.py:38
  432.4 29.2 %collective-permute-start.15 = (bf16[512,640]{1,0:T(8,128)(2,1)S(1)}, bf16[512,640]{1,0:T(8,128)(2,1)S(1)}, u32[]{:S(2)}, u32[]{:S(2)}) collective-permute-start(bf16[512,640]{1,0:T(8,128)(2,1)S(1)} %fusion.37), channel_id=1, source_target_pairs={{0,1},{1,0},{2,3},{3,2},{4,5},{5,4},{6,7},{7,6},{8,9},{9,8},{10,11... | collective-permute-start | bytes 1966088 | tf_op jit(solution)/shard_map/ppermute | solution.py:38
  433.9 27.6 %copy-start.54 = (bf16[2,512,640]{2,1,0:T(8,128)(2,1)}, bf16[2,512,640]{2,1,0:T(8,128)(2,1)S(1)}, u32[]{:S(2)}) copy-start(bf16[2,512,640]{2,1,0:T(8,128)(2,1)S(1)} %collective-permute-done.12) | copy-start | bytes 3932164
  435.1 26.7 %collective-permute-start.13 = (bf16[512,640]{1,0:T(8,128)(2,1)}, bf16[512,640]{1,0:T(8,128)(2,1)}, u32[]{:S(2)}, u32[]{:S(2)}) collective-permute-start(bf16[512,640]{1,0:T(8,128)(2,1)} %fusion.36), channel_id=1, source_target_pairs={{0,2},{1,3},{2,0},{3,1},{4,6},{5,7},{6,4},{7,5},{8,10},{9,11},{10,... | collective-permute-start | bytes 1966088 | tf_op jit(solution)/shard_map/ppermute | solution.py:38
  462.8 49.8 %slice-start = ((s8[7208960]{0:T(1024)(128)(4,1)}), s8[4194304]{0:T(1024)(128)(4,1)S(1)}, s32[]{:S(2)}) async-start(s8[7208960]{0:T(1024)(128)(4,1)} %bitcast.126), calls=%async_computation.14 | async-start | bytes 8388608
  464.4 48.2 %slice-start.1 = ((s8[7208960]{0:T(1024)(128)(4,1)}), s8[3014656]{0:T(1024)(128)(4,1)S(1)}, s32[]{:S(2)}) async-start(s8[7208960]{0:T(1024)(128)(4,1)} %bitcast.126), calls=%async_computation.15 | async-start | bytes 6029312
  468.3 28.9 %collective-permute-start.20 = (bf16[1024,640]{1,0:T(8,128)(2,1)S(1)}, bf16[1024,640]{1,0:T(8,128)(2,1)S(1)}, u32[]{:S(2)}, u32[]{:S(2)}) collective-permute-start(bf16[1024,640]{1,0:T(8,128)(2,1)S(1)} %get-tuple-element.79.refs_0_), channel_id=1, source_target_pairs={{0,2},{1,3},{2,0},{3,1},{4,6},{5,7},{6,4},{7,5},{8,10},{9,11},{10,... | collective-permute-start | bytes 3932168 | tf_op jit(solution)/shard_map/ppermute | solution.py:38
  468.9 29.6 %collective-permute-start.19 = (bf16[1024,640]{1,0:T(8,128)(2,1)S(1)}, bf16[1024,640]{1,0:T(8,128)(2,1)S(1)}, u32[]{:S(2)}, u32[]{:S(2)}) collective-permute-start(bf16[1024,640]{1,0:T(8,128)(2,1)S(1)} %get-tuple-element.79.refs_0_), channel_id=1, source_target_pairs={{0,1},{1,0},{2,3},{3,2},{4,5},{5,4},{6,7},{7,6},{8,9},{9,8},{10,11... | collective-permute-start | bytes 3932168 | tf_op jit(solution)/shard_map/ppermute | solution.py:38
  469.7 66.7 %collective-permute-start.43 = (bf16[1280,2688]{1,0:T(8,128)(2,1)}, bf16[1280,2688]{1,0:T(8,128)(2,1)}, u32[]{:S(2)}, u32[]{:S(2)}) collective-permute-start(bf16[1280,2688]{1,0:T(8,128)(2,1)} %get-tuple-element.105), channel_id=1, source_target_pairs={{0,4},{4,0},{8,12},{12,8},{16,20},{20,16},{24,28},{28,24},{1,5},{5... | collective-permute-start | bytes 20643848 | tf_op jit(solution)/shard_map/ppermute | solution.py:780
  497.3 14.3 %collective-permute-start.22 = (bf16[512,640]{1,0:T(8,128)(2,1)S(1)}, bf16[512,640]{1,0:T(8,128)(2,1)S(1)}, u32[]{:S(2)}, u32[]{:S(2)}) collective-permute-start(bf16[512,640]{1,0:T(8,128)(2,1)S(1)} %slice.285), channel_id=1, source_target_pairs={{0,1},{1,0},{2,3},{3,2},{4,5},{5,4},{6,7},{7,6},{8,9},{9,8},{10,11... | collective-permute-start | bytes 1966088 | tf_op jit(solution)/shard_map/ppermute | solution.py:38
  498.5 14.1 %collective-permute-start.21 = (bf16[512,640]{1,0:T(8,128)(2,1)S(1)}, bf16[512,640]{1,0:T(8,128)(2,1)S(1)}, u32[]{:S(2)}, u32[]{:S(2)}) collective-permute-start(bf16[512,640]{1,0:T(8,128)(2,1)S(1)} %slice.284), channel_id=1, source_target_pairs={{0,2},{1,3},{2,0},{3,1},{4,6},{5,7},{6,4},{7,5},{8,10},{9,11},{10,... | collective-permute-start | bytes 1966088 | tf_op jit(solution)/shard_map/ppermute | solution.py:38
  527.6 3.7 collective-permute-start.42
  536.3 263.4 %reduce-scatter.9.cloned.1.call-start = ((), (), s32[]{:S(2)}) async-start(), calls=%async_computation.12 | async-start | bytes 8601600 | tf_op jit(solution)/shard_map/reduce_scatter | solution.py:783
  549.1 281.7 %reduce-scatter.11.cloned.1.call-start = ((), (), s32[]{:S(2)}) async-start(), calls=%async_computation.13 | async-start | bytes 9830400 | tf_op jit(solution)/shard_map/reduce_scatter | solution.py:783
  549.1 12.7 %collective-permute-start.44 = (bf16[1280,3072]{1,0:T(8,128)(2,1)}, bf16[1280,3072]{1,0:T(8,128)(2,1)S(1)}, u32[]{:S(2)}, u32[]{:S(2)}) collective-permute-start(bf16[1280,3072]{1,0:T(8,128)(2,1)} %get-tuple-element.106), channel_id=1, source_target_pairs={{0,4},{4,0},{8,12},{12,8},{16,20},{20,16},{24,28},{28,24},{1,5},{5... | collective-permute-start | bytes 23592968 | tf_op jit(solution)/shard_map/ppermute | solution.py:780
  570.1 21.9 %all-to-all-start.2 = ((bf16[4,256,640]{2,1,0:T(8,128)(2,1)}), bf16[4,256,640]{2,1,0:T(8,128)(2,1)}, u32[]{:S(2)}, u32[]{:S(2)}) async-start(bf16[4,256,640]{2,1,0:T(8,128)(2,1)} %bitcast.24), calls=%async_computation.2 | async-start | bytes 2621440 | tf_op jit(solution)/shard_map/all_to_all | solution.py:144
  612.2 7.6 collective-permute-start.23
  614.4 7.5 collective-permute-start.25
  620.5 5.2 collective-permute-start.24
  627.5 5.2 collective-permute-start.26
  637.0 39.8 %all-to-all-start.3 = ((bf16[256,4,768]{2,0,1:T(8,128)(2,1)}), bf16[256,4,768]{2,0,1:T(8,128)(2,1)}, u32[]{:S(2)}, u32[]{:S(2)}) async-start(bf16[256,4,768]{2,0,1:T(8,128)(2,1)} %bitcast.124), calls=%async_computation.3 | async-start | bytes 3145728 | tf_op jit(solution)/shard_map/all_to_all | solution.py:148
  641.3 234.2 %reduce-scatter.5.cloned.1.call-start = ((), (), s32[]{:S(2)}) async-start(), calls=%async_computation.10 | async-start | bytes 2457600 | tf_op jit(solution)/shard_map/reduce_scatter | solution.py:783
  674.9 30.8 %collective-permute-start.18 = (bf16[2,512,640]{2,1,0:T(8,128)(2,1)}, bf16[2,512,640]{2,1,0:T(8,128)(2,1)}, u32[]{:S(2)}, u32[]{:S(2)}) collective-permute-start(bf16[2,512,640]{2,1,0:T(8,128)(2,1)} %get-tuple-element.83), channel_id=1, source_target_pairs={{0,1},{1,0},{2,3},{3,2},{4,5},{5,4},{6,7},{7,6},{8,9},{9,8},{10,11... | collective-permute-start | bytes 3932168 | tf_op jit(solution)/shard_map/ppermute | solution.py:38
  699.7 42.9 %collective-permute-start.41 = (bf16[1280,768]{1,0:T(8,128)(2,1)}, bf16[1280,768]{1,0:T(8,128)(2,1)}, u32[]{:S(2)}, u32[]{:S(2)}) collective-permute-start(bf16[1280,768]{1,0:T(8,128)(2,1)} %get-tuple-element.100), channel_id=1, source_target_pairs={{0,4},{4,0},{8,12},{12,8},{16,20},{20,16},{24,28},{28,24},{1,5},{5... | collective-permute-start | bytes 5898248 | tf_op jit(solution)/shard_map/ppermute | solution.py:780
  699.7 32.0 %collective-permute-start.28 = (bf16[2,512,640]{2,1,0:T(8,128)(2,1)}, bf16[2,512,640]{2,1,0:T(8,128)(2,1)}, u32[]{:S(2)}, u32[]{:S(2)}) collective-permute-start(bf16[2,512,640]{2,1,0:T(8,128)(2,1)} %get-tuple-element.89), channel_id=1, source_target_pairs={{0,2},{1,3},{2,0},{3,1},{4,6},{5,7},{6,4},{7,5},{8,10},{9,11},{10,... | collective-permute-start | bytes 3932168 | tf_op jit(solution)/shard_map/ppermute | solution.py:38
  701.7 30.0 %copy-start.10 = (bf16[2,512,640]{2,1,0:T(8,128)(2,1)S(1)}, bf16[2,512,640]{2,1,0:T(8,128)(2,1)}, u32[]{:S(2)}) copy-start(bf16[2,512,640]{2,1,0:T(8,128)(2,1)} %copy-done.9) | copy-start | bytes 3932164
  701.7 3.8 collective-permute-start.36
  704.4 57.9 %collective-permute-start.32 = (bf16[2,512,640]{2,1,0:T(8,128)(2,1)}, bf16[2,512,640]{2,1,0:T(8,128)(2,1)}, u32[]{:S(2)}, u32[]{:S(2)}) collective-permute-start(bf16[2,512,640]{2,1,0:T(8,128)(2,1)} %get-tuple-element.95), channel_id=1, source_target_pairs={{0,2},{1,3},{2,0},{3,1},{4,6},{5,7},{6,4},{7,5},{8,10},{9,11},{10,... | collective-permute-start | bytes 3932168 | tf_op jit(solution)/shard_map/ppermute | solution.py:38
  705.6 4.2 collective-permute-start.37
  705.7 7.9 collective-permute-start.34
  709.8 55.4 %collective-permute-start.30 = (bf16[2,512,640]{2,1,0:T(8,128)(2,1)}, bf16[2,512,640]{2,1,0:T(8,128)(2,1)}, u32[]{:S(2)}, u32[]{:S(2)}) collective-permute-start(bf16[2,512,640]{2,1,0:T(8,128)(2,1)} %copy-done.28), channel_id=1, source_target_pairs={{0,1},{1,0},{2,3},{3,2},{4,5},{5,4},{6,7},{7,6},{8,9},{9,8},{10,11... | collective-permute-start | bytes 3932168 | tf_op jit(solution)/shard_map/ppermute | solution.py:38
  713.5 7.3 collective-permute-start.38
  720.9 38.6 %collective-permute-start.35 = (f32[4,256]{1,0:T(4,128)S(1)}, f32[4,256]{1,0:T(4,128)S(1)}, u32[]{:S(2)}, u32[]{:S(2)}) collective-permute-start(f32[4,256]{1,0:T(4,128)S(1)} %add.420), channel_id=1, source_target_pairs={{0,2},{1,3},{2,0},{3,1},{4,6},{5,7},{6,4},{7,5},{8,10},{9,11},{10,... | collective-permute-start | bytes 12296 | tf_op jit(solution)/shard_map/ppermute | solution.py:38
  731.7 9.4 %collective-permute-start.39 = (f32[8,320]{1,0:T(8,128)S(1)}, f32[8,320]{1,0:T(8,128)S(1)}, u32[]{:S(2)}, u32[]{:S(2)}) collective-permute-start(f32[8,320]{1,0:T(8,128)S(1)} %add.425), channel_id=1, source_target_pairs={{0,1},{1,0},{2,3},{3,2},{4,5},{5,4},{6,7},{7,6},{8,9},{9,8},{10,11... | collective-permute-start | bytes 30728 | tf_op jit(solution)/shard_map/ppermute | solution.py:38
  741.1 20.4 %collective-permute-start.40 = (f32[8,320]{1,0:T(8,128)S(1)}, f32[8,320]{1,0:T(8,128)S(1)}, u32[]{:S(2)}, u32[]{:S(2)}) collective-permute-start(f32[8,320]{1,0:T(8,128)S(1)} %add.426), channel_id=1, source_target_pairs={{0,2},{1,3},{2,0},{3,1},{4,6},{5,7},{6,4},{7,5},{8,10},{9,11},{10,... | collective-permute-start | bytes 30728 | tf_op jit(solution)/shard_map/ppermute | solution.py:38
  759.5 17.9 %collective-permute-start.27 = (bf16[512,640]{1,0:T(8,128)(2,1)}, bf16[512,640]{1,0:T(8,128)(2,1)}, u32[]{:S(2)}, u32[]{:S(2)}) collective-permute-start(bf16[512,640]{1,0:T(8,128)(2,1)} %fusion.38), channel_id=1, source_target_pairs={{0,2},{1,3},{2,0},{3,1},{4,6},{5,7},{6,4},{7,5},{8,10},{9,11},{10,... | collective-permute-start | bytes 1966088 | tf_op jit(solution)/shard_map/ppermute | solution.py:38
  761.0 18.0 %collective-permute-start.29 = (bf16[512,640]{1,0:T(8,128)(2,1)}, bf16[512,640]{1,0:T(8,128)(2,1)S(1)}, u32[]{:S(2)}, u32[]{:S(2)}) collective-permute-start(bf16[512,640]{1,0:T(8,128)(2,1)} %fusion.39), channel_id=1, source_target_pairs={{0,1},{1,0},{2,3},{3,2},{4,5},{5,4},{6,7},{7,6},{8,9},{9,8},{10,11... | collective-permute-start | bytes 1966088 | tf_op jit(solution)/shard_map/ppermute | solution.py:38
  763.7 27.3 %collective-permute-start.33 = (bf16[512,640]{1,0:T(8,128)(2,1)S(1)}, bf16[512,640]{1,0:T(8,128)(2,1)S(1)}, u32[]{:S(2)}, u32[]{:S(2)}) collective-permute-start(bf16[512,640]{1,0:T(8,128)(2,1)S(1)} %fusion.41), channel_id=1, source_target_pairs={{0,1},{1,0},{2,3},{3,2},{4,5},{5,4},{6,7},{7,6},{8,9},{9,8},{10,11... | collective-permute-start | bytes 1966088 | tf_op jit(solution)/shard_map/ppermute | solution.py:38
  766.5 26.1 %collective-permute-start.31 = (bf16[512,640]{1,0:T(8,128)(2,1)S(1)}, bf16[512,640]{1,0:T(8,128)(2,1)S(1)}, u32[]{:S(2)}, u32[]{:S(2)}) collective-permute-start(bf16[512,640]{1,0:T(8,128)(2,1)S(1)} %fusion.40), channel_id=1, source_target_pairs={{0,2},{1,3},{2,0},{3,1},{4,6},{5,7},{6,4},{7,5},{8,10},{9,11},{10,... | collective-permute-start | bytes 1966088 | tf_op jit(solution)/shard_map/ppermute | solution.py:38
  803.0 29.9 %copy-start.47 = (bf16[320,1920]{1,0:T(8,128)(2,1)S(1)}, bf16[320,1920]{1,0:T(8,128)(2,1)}, u32[]{:S(2)}) copy-start(bf16[320,1920]{1,0:T(8,128)(2,1)} %refs_0_.1) | copy-start | bytes 3686404
  836.3 41.4 %collective-permute-start.45 = (f32[320]{0:T(512)S(1)}, f32[320]{0:T(512)S(1)}, u32[]{:S(2)}, u32[]{:S(2)}) collective-permute-start(f32[320]{0:T(512)S(1)} %get-tuple-element.122), channel_id=1, source_target_pairs={{0,1},{1,0},{2,3},{3,2},{4,5},{5,4},{6,7},{7,6},{8,9},{9,8},{10,11... | collective-permute-start | bytes 3848 | tf_op jit(solution)/shard_map/ppermute | solution.py:38
  877.7 4.3 collective-permute-start.46
  (67 other events, 564.7 us)
Sparse Core Ops, SparseCore 0:
  79.1 126.5 all-gather.2
  207.3 140.6 all-gather.4
  536.5 33.2 reduce-scatter.6
  572.0 119.2 reduce-scatter.8
  693.4 137.3 reduce-scatter.10
  833.5 42.0 reduce-scatter.4

commit v12 on v11

--- a/solution.py
+++ b/solution.py
@@ -148,15 +148,15 @@
     return lax.all_to_all(block, "mdl", split_axis=1, concat_axis=0, tiled=True)
 
 
-def first_kernel(parts, x_ref, w_ref, *refs):
-    weights, (rows_ref, weight_ref), locals_ref = refs[:3], refs[3:5], refs[5:7]
-    held, joined = refs[7:10], refs[10:12]
-    own, x_sent, x_got, w_up, w_down, w_core, w_got = refs[12:]
+def first_kernel(parts, x_ref, gains_ref, right_ref, *refs):
+    weights, (rows_ref, weight_ref), locals_ref = refs[:4], refs[4:6], refs[6:8]
+    held, joined, left_ref = refs[8:12], refs[12:14], refs[14]
+    own, x_sent, x_got, w_up, w_down, w_core, w_got = refs[15:]
     me, tok = lax.axis_index("mdl"), lax.axis_index("tok")
     pairs = lax.axis_size("tok") // 2
     level, last = tok // 2, pairs - 1
     half, width = x_ref.shape[0] // 2, x_ref.shape[1]
-    shard, all_cols = w_ref.shape[0], weight_ref.shape[1]
+    shard, split, all_cols = *left_ref.shape, weight_ref.shape[1]
     below, above = level > 0, level < last
 
     barrier = pltpu.get_barrier_semaphore()
@@ -177,10 +177,10 @@
     def cols(block):
         return pl.ds(pl.multiple_of(block * width, 128), width)
 
-    piece = shard // 2
+    windows = (pl.ds(split, all_cols - split), pl.ds(0, split))
 
     def block(index, part):
-        return weight_ref.at[pl.ds(pl.multiple_of(index * shard + part * piece, 16), piece)]
+        return weight_ref.at[pl.ds(pl.multiple_of(index * shard, 16), shard), windows[part]]
 
     def x_copy(source, target, at, to):
         return pltpu.make_async_remote_copy(
@@ -195,31 +195,33 @@
     mine = rows_ref.at[:, cols(me)]
     to_x, to_y = x_copy(x_ref, mine, 0, 1), x_copy(x_ref, mine, 1, 2)
     keeps = [pltpu.make_async_copy(x_ref, mine, own.at[0])]
-    for part in range(2):
-        source = w_ref.at[pl.ds(part * piece, piece), pl.ds(0, all_cols)]
-
-        @pl.when(above)
-        def _(source=source, part=part):
-            w_copy(source, tok, part, w_up.at[0, part], tok + 2).start()
-
-        @pl.when(below)
-        def _(source=source, part=part):
-            w_copy(source, tok, part, w_down.at[0, part], tok - 2).start()
-
-        w_copy(source, tok, part, w_core.at[tok, part], tok ^ 1).start()
-        keeps.append(pltpu.make_async_copy(source, block(tok, part), own.at[1 + part]))
-        if part == 0:
-            to_x.start()
-            to_y.start()
     loads = [
         pltpu.make_async_copy(weight, to, own.at[3 + at])
         for at, (weight, to) in enumerate(zip(weights, held))
     ]
-    for copy in (*keeps, *loads):
+
+    def send_own(source, part):
+        @pl.when(above)
+        def _():
+            w_copy(source, tok, part, w_up.at[0, part], tok + 2).start()
+
+        @pl.when(below)
+        def _():
+            w_copy(source, tok, part, w_down.at[0, part], tok - 2).start()
+
+        w_copy(source, tok, part, w_core.at[tok, part], tok ^ 1).start()
+        keeps.append(pltpu.make_async_copy(source, block(tok, part), own.at[1 + part]))
+        keeps[-1].start()
+
+    send_own(right_ref, 0)
+    for copy in (to_x, to_y, keeps[0], *loads):
         copy.start()
-    for copy in loads:
+    loads[0].wait()
+    gain_one, gain = gains_ref[:, :1].astype(F32), gains_ref[:, 64:65].astype(F32)
+    left_ref[...] = (held[0][...].astype(F32) * gain_one).astype(BF16)
+    held = held[1:]
+    for copy in loads[1:]:
         copy.wait()
-    gain = w_ref[:, all_cols : all_cols + 1].astype(F32)
     for (start, stop), out in zip(parts, joined):
         count = stop - start
         for at, source in enumerate(held):
@@ -227,6 +229,8 @@
             if at < 2:
                 value = (value.astype(F32) * gain).astype(BF16)
             out[:, at * count : (at + 1) * count] = value
+        if start == 0:
+            send_own(left_ref, 1)
 
     def relay(distance, part):
         low, high = tok - 2 * distance, tok + 2 * distance
@@ -256,7 +260,7 @@
     relay(1, 0)
     relay(1, 1)
     stores = [
-        pltpu.make_async_copy(out, to, own.at[6 + at])
+        pltpu.make_async_copy(out, to, own.at[7 + at])
         for at, (out, to) in enumerate(zip(joined, locals_ref))
     ]
     for copy in stores:
@@ -295,29 +299,30 @@
             w_copy(block(far, part), far, part, w_core.at[near, part], tok ^ 1).wait_recv()
 
 
-def first_gather(inputs, weight, weights, parts):
+def first_gather(inputs, gains, right, weights, parts):
     tokens, width = inputs.shape
-    shard, cols = weight.shape
+    shard, left_cols = weights[0].shape
+    cols = left_cols + right.shape[1]
     pairs = lax.axis_size("tok") // 2
     dma = pltpu.SemaphoreType.DMA
     locals_ff = [(shard, 3 * (stop - start)) for start, stop in parts]
-    shapes = [(tokens, 4 * width), (2 * pairs * shard, cols - 128), *locals_ff]
+    shapes = [(tokens, 4 * width), (2 * pairs * shard, cols), *locals_ff]
     *gathered, first, second = pl.pallas_call(
         functools.partial(first_kernel, parts),
         out_shape=[jax.ShapeDtypeStruct(shape, BF16) for shape in shapes],
-        in_specs=[pl.BlockSpec(memory_space=pltpu.VMEM)] * 2
-        + [pl.BlockSpec(memory_space=pl.ANY)] * 3,
+        in_specs=[pl.BlockSpec(memory_space=pltpu.VMEM)] * 3
+        + [pl.BlockSpec(memory_space=pl.ANY)] * 4,
         out_specs=[pl.BlockSpec(memory_space=pl.ANY)] * 4,
         scratch_shapes=[pltpu.VMEM(array.shape, BF16) for array in weights]
-        + [pltpu.VMEM(shape, BF16) for shape in locals_ff]
+        + [pltpu.VMEM(shape, BF16) for shape in (*locals_ff, weights[0].shape)]
         + [
-            dma((8,)), dma((4,)), dma((4,)), dma((pairs, 2)), dma((pairs, 2)),
+            dma((9,)), dma((4,)), dma((4,)), dma((pairs, 2)), dma((pairs, 2)),
             dma((2 * pairs, 2)), dma((2 * pairs, 2)),
         ],
         compiler_params=pltpu.CompilerParams(
             collective_id=0, has_side_effects=True, vmem_limit_bytes=60 << 20
         ),
-    )(inputs, weight, *weights)
+    )(inputs, gains, right, *weights)
     return *gathered, (first, second)
 
 
@@ -786,19 +791,20 @@
         return total.astype(F32)
 
     qkv_cols, ff_cols = qkv_weight.shape[1], gate_weight.shape[1]
-    attn_local = jnp.concatenate([scaled(qkv_weight, norm1_gain), out_weight.T], axis=1)
     middle = ff_cols // 256 * 128
     parts = ((0, middle), (middle, ff_cols))
     if size == 4 and lax.axis_size("tok") == 8:
-        gain_cols = jnp.broadcast_to(norm2_gain[:, None], (norm2_gain.shape[0], 128))
+        lane = lax.broadcasted_iota(jnp.int32, (norm1_gain.shape[0], 128), 1)
         rows_in, w_attn, locals_ff = first_gather(
             inputs,
-            jnp.concatenate([attn_local, gain_cols], axis=1),
-            (gate_weight, up_weight, down_weight.T),
+            jnp.where(lane < 64, norm1_gain[:, None], norm2_gain[:, None]),
+            out_weight.T,
+            (qkv_weight, gate_weight, up_weight, down_weight.T),
             parts,
         )
     else:
         rows_in = gather_mdl(inputs, 1)
+        attn_local = jnp.concatenate([scaled(qkv_weight, norm1_gain), out_weight.T], axis=1)
         w_attn = from_tok(attn_local, 0)
         scaled_gu = [scaled(weight, norm2_gain) for weight in (gate_weight, up_weight)]
         locals_ff = [

time: 898 us -> 894 us (level)
  no operation moved by 1% of the time
where the time goes in v12:
time: 894 us; the launch traced here: 886 us
  waiting for transfers between devices  342 us (38%)
  Pallas kernels  264 us (30%)
  other arithmetic  69 us (8%)
  matrix products  68.5 us (8%)
  starting transfers between devices  58.9 us (7%)
  local copies, waits for them, and re-layouts  49.8 us (6%)
  blocking collectives  18.5 us (2%)
  between operations  15.3 us (2%)
    ppermute x40, waiting for transfers between devices, swap(): return lax.ppermute(block, 'mdl', [(i, i ^ distance) for i in range(size)])  204 us
    dot_general x7, matrix products, nn(): return jnp.dot(left_op, right_op, preferred_element_type=F32)  68.5 us
    pallas_call x1, Pallas kernels, first_gather(): pl.pallas_call(functools.partial(first_kernel, parts), out_shape=[jax.Sha...  66.9 us
    reduce_scatter x4, waiting for transfers between devices, pair_to_tok(): lax.psum_scatter(both, 'tok', scatter_dimension=0, tiled=True, axis_index...  65.6 us
    pallas_call x4, Pallas kernels, scatter_product(): pl.pallas_call(functools.partial(payload_kernel, starts), grid_spec=pltpu...  50 us
    pallas_call x2, Pallas kernels, part_grad(): pl.pallas_call(part_kernel, grid=(pairs,), out_shape=(out, out), in_specs...  48.5 us
    ppermute x40, starting transfers between devices, swap(): return lax.ppermute(block, 'mdl', [(i, i ^ distance) for i in range(size)])  45.3 us
    all_to_all x2, waiting for transfers between devices, rows_to_cols(): return lax.all_to_all(block, 'mdl', split_axis=0, concat_axis=1, tiled=True)  35.3 us
  transfers between devices with their start and end apart: 56, of which 30 were waited for; matrix products, arithmetic and copies ran while one was open for 13% of the time, Pallas kernels for 20%

profile of v12, /device:TPU:0, one launch (start us, length us, event | category | flops | bytes accessed | tf_op | source)
XLA Modules:
  0.0 886.4 jit_solution(14620653631722294219)
XLA Ops:
  8.7 66.9 %shard_map.169 = (bf16[1024,2560]{1,0:T(8,128)(2,1)}, bf16[2560,1408]{1,0:T(8,128)(2,1)}, bf16[320,2688]{1,0:T(8,128)(2,1)}, bf16[320,3072]{1,0:T(8,128)(2,1)}) custom-call(bf16[1024,640]{1,0:T(8,128)(2,1)} %x_ref.1, bf16[320,128]{1,0:T(8,128)(2,1)} %broadcast_select_fusion.gains_ref, bf16[320,640]{1,0:T(8,128)(2,1)} %bitcast.142, bf16[320,768]{1,0:T(8,128)(2,1)} %refs_0_.1, ...), custom_call_target="tpu_custom_call" | custom-call | tf_op jit(solution)/shard_map/pallas_call | solution.py:310
  76.4 9.0 %fusion.30 = bf16[1024,768]{1,0:T(8,128)(2,1)} fusion(bf16[1024,2560]{1,0:T(8,128)(2,1)} %get-tuple-element.91.left_ref, bf16[2560,1408]{1,0:T(8,128)(2,1)} %get-tuple-element.60.refs_1_.refs_5_.refs_0_), kind=kOutput, calls=%fused_computation.57 | convolution fusion | flops 4027318272 | bytes 10747904 | tf_op jit(solution)/shard_map/dot_general | solution.py:33
  85.5 3.8 all-to-all-start
  91.1 18.2 %all-to-all-done = bf16[4,256,768]{2,1,0:T(8,128)(2,1)S(1)} async-done(((bf16[4,256,768]{2,1,0:T(8,128)(2,1)}), bf16[4,256,768]{2,1,0:T(8,128)(2,1)S(1)}, u32[]{:S(2)}, u32[]{:S(2)}) %all-to-all-start) | async-done | bytes 1572896 | tf_op jit(solution)/shard_map/all_to_all | solution.py:144
  114.2 5.6 collective-permute-done
  127.3 11.2 %att_f.1 = (bf16[256,2560]{1,0:T(8,128)(2,1)S(1)}, f32[10,256,1]{2,1,0:T(8,128)S(1)}) custom-call(s32[1]{0:T(128)} %bitcast.1.first_ref, bf16[256,3072]{1,0:T(8,128)(2,1)S(1)} %bitcast.129, bf16[1024,512]{1,0:T(8,128)(2,1)S(1)} %constant_dynamic-update-slice_fusion.4.kv_ref, f32[256,128]{1,0:T(8,128)S(1)} %get-tuple-element.145.cos_ref, ...), custom_call_target="tpu_custom_call" | custom-call | flops 2684354560 | bytes 3670016 | tf_op jit(solution)/shard_map/att_f/pallas_call | solution.py:407
  138.7 18.5 %all_to_all.76 = bf16[256,4,640]{2,0,1:T(8,128)(2,1)} all-to-all(bf16[256,4,640]{2,0,1:T(8,128)(2,1)S(1)} %bitcast.138), channel_id=1, replica_groups=mesh['tok'=8,'mdl'=4] {'mdl'}, dimensions={1} | all-to-all | bytes 2621440 | tf_op jit(solution)/shard_map/all_to_all | solution.py:148
  157.2 7.9 shard_map.170
  166.7 25.7 %collective-permute-done.4 = bf16[2,512,640]{2,1,0:T(8,128)(2,1)S(1)} collective-permute-done((bf16[2,512,640]{2,1,0:T(8,128)(2,1)S(1)}, bf16[2,512,640]{2,1,0:T(8,128)(2,1)S(1)}, u32[]{:S(2)}, u32[]{:S(2)}) %collective-permute-start.4) | collective-permute-done | bytes 1310752 | tf_op jit(solution)/shard_map/ppermute | solution.py:38
  197.4 10.1 %collective-permute-done.5 = bf16[512,640]{1,0:T(8,128)(2,1)S(1)} collective-permute-done((bf16[512,640]{1,0:T(8,128)(2,1)}, bf16[512,640]{1,0:T(8,128)(2,1)S(1)}, u32[]{:S(2)}, u32[]{:S(2)}) %collective-permute-start.5) | collective-permute-done | bytes 655392 | tf_op jit(solution)/shard_map/ppermute | solution.py:38
  211.1 3.5 broadcast_in_dim.43
  218.0 24.4 %collective-permute-done.8 = bf16[1024,640]{1,0:T(8,128)(2,1)S(1)} collective-permute-done((bf16[1024,640]{1,0:T(8,128)(2,1)S(1)}, bf16[1024,640]{1,0:T(8,128)(2,1)S(1)}, u32[]{:S(2)}, u32[]{:S(2)}) %collective-permute-start.8) | collective-permute-done | bytes 1310752 | tf_op jit(solution)/shard_map/ppermute | solution.py:38
  251.8 4.8 collective-permute-done.10
  259.6 3.6 fusion
  263.2 5.8 fusion.1.rows_ref
  269.0 9.7 %fusion.12 = f32[896,1024]{0,1:T(8,128)S(1)} fusion(bf16[1024,2560]{1,0:T(8,128)(2,1)} %above_ref.2, bf16[2560,2688]{1,0:T(8,128)(2,1)} %all-gather.3.cloned.1.call-done.refs_2_.refs_1_), kind=kOutput, calls=%fused_computation.15 | convolution fusion | flops 4697620480 | bytes 13500416 | tf_op jit(solution)/shard_map/dot_general | solution.py:33
  278.6 7.9 fusion.8
  286.5 9.3 %add_reduce_fusion.1 = (f32[1024]{0:T(1024)S(1)}, bf16[1024,896]{1,0:T(8,128)(2,1)S(1)}, bf16[1024,896]{1,0:T(8,128)(2,1)S(1)}, bf16[1024,896]{1,0:T(8,128)(2,1)S(1)}) fusion(f32[1024,896]{1,0:T(8,128)S(1)} %fusion.8, f32[896,1024]{0,1:T(8,128)S(1)} %fusion.12, bf16[1024,2560]{1,0:T(8,128)(2,1)S(1)} %copy-done.46, ...), kind=kOutput, calls=%fused_computation.29 | convolution fusion | flops 4723309568 | bytes 22679552 | tf_op jit(solution)/shard_map/dot_general | solution.py:33
  295.9 23.6 %shard_map.171 = (bf16[1280,2688]{1,0:T(8,128)(2,1)}, bf16[1280,2688]{1,0:T(8,128)(2,1)}) custom-call(s32[1]{0:T(128)} %bitcast.14.core_ref, bf16[1024,2560]{1,0:T(8,128)(2,1)} %fusion.1.rows_ref, bf16[1024,2560]{1,0:T(8,128)(2,1)} %above_ref.2, bf16[1024,896]{1,0:T(8,128)(2,1)S(1)} %get-tuple-element.71.d_gate_ref.refs_0_, ...), custom_call_target="tpu_custom_call" | custom-call | flops 14092861440 | bytes 29753344 | tf_op jit(solution)/shard_map/pallas_call | solution.py:547
  319.5 15.3 %shard_map.172.refs_3_ = f32[1024,2560]{1,0:T(8,128)} custom-call(bf16[1024,896]{1,0:T(8,128)(2,1)S(1)} %get-tuple-element.71.d_gate_ref.refs_0_, bf16[1024,896]{1,0:T(8,128)(2,1)S(1)} %get-tuple-element.119.d_up_ref.refs_1_, bf16[2560,2688]{1,0:T(8,128)(2,1)} %all-gather.3.cloned.1.call-done.refs_2_.refs_1_), custom_call_target="tpu_custom_call" | custom-call | flops 9395240960 | bytes 24248320 | tf_op jit(solution)/shard_map/pallas_call | solution.py:648
  334.7 10.0 %all-gather.5.cloned.1.call-done.refs_2_.refs_1_ = bf16[2560,3072]{1,0:T(8,128)(2,1)} async-done(((bf16[320,3072]{1,0:T(8,128)(2,1)}), bf16[2560,3072]{1,0:T(8,128)(2,1)}) %all-gather.5.cloned.1.call-update) | async-done | bytes 15728656 | tf_op jit(solution)/shard_map/all_gather | solution.py:780
  344.7 10.7 %fusion.2 = f32[1024,1024]{1,0:T(8,128)} fusion(bf16[1024,2560]{1,0:T(8,128)(2,1)} %above_ref.2, bf16[2560,3072]{1,0:T(8,128)(2,1)} %all-gather.5.cloned.1.call-done.refs_2_.refs_1_), kind=kOutput, calls=%fused_computation.5 | convolution fusion | flops 5368709120 | bytes 14680064 | tf_op jit(solution)/shard_map/dot_general | solution.py:33
  355.4 8.9 %fusion.4 = f32[1024,1024]{1,0:T(8,128)} fusion(bf16[1024,2560]{1,0:T(8,128)(2,1)} %fusion.1.rows_ref, bf16[2560,3072]{1,0:T(8,128)(2,1)S(1)} %copy-done.42), kind=kOutput, calls=%fused_computation.7 | convolution fusion | flops 5368709120 | bytes 14680064 | tf_op jit(solution)/shard_map/dot_general | solution.py:33
  364.4 13.0 %fusion.67 = (bf16[1024,1024]{1,0:T(8,128)(2,1)}, f32[1024]{0:T(1024)S(1)}, bf16[1024,1024]{1,0:T(8,128)(2,1)}, bf16[1024,1024]{1,0:T(8,128)(2,1)}) fusion(f32[1024,1024]{1,0:T(8,128)} %fusion.2, f32[1024,1024]{1,0:T(8,128)} %fusion.4, bf16[1024,2560]{1,0:T(8,128)(2,1)S(1)} %bitcast.137, bf16[2560,3072]{1,0:T(8,128)(2,1)S(1)} %copy-done.42), kind=kOutput, calls=%fused_computation.158 | convolution fusion | flops 5398068224 | bytes 25169920 | tf_op jit(solution)/shard_map/dot_general | solution.py:33
  377.3 18.7 %shard_map.173 = (bf16[2,512,640]{2,1,0:T(8,128)(2,1)S(1)}, bf16[2,512,640]{2,1,0:T(8,128)(2,1)S(1)}, bf16[2,512,640]{2,1,0:T(8,128)(2,1)S(1)}, bf16[2,512,640]{2,1,0:T(8,128)(2,1)S(1)}) custom-call(s32[1]{0:T(128)} %bitcast.me_ref, bf16[1024,1024]{1,0:T(8,128)(2,1)} %get-tuple-element.113.refs_0_.d_gate_ref, ...), custom_call_target="tpu_custom_call" | custom-call | flops 10737418240 | bytes 25165824 | tf_op jit(solution)/shard_map/pallas_call | solution.py:689
  399.7 28.7 %collective-permute-done.16 = f32[8,128]{1,0:T(8,128)S(1)} collective-permute-done((f32[8,128]{1,0:T(8,128)S(1)}, f32[8,128]{1,0:T(8,128)S(1)}, u32[]{:S(2)}, u32[]{:S(2)}) %collective-permute-start.16) | collective-permute-done | bytes 4128 | tf_op jit(solution)/shard_map/ppermute | solution.py:38
  433.3 24.9 %shard_map.174 = (bf16[1280,3072]{1,0:T(8,128)(2,1)}, bf16[1280,3072]{1,0:T(8,128)(2,1)}) custom-call(s32[1]{0:T(128)} %bitcast.14.core_ref, bf16[1024,2560]{1,0:T(8,128)(2,1)} %fusion.1.rows_ref, bf16[1024,2560]{1,0:T(8,128)(2,1)} %above_ref.2, bf16[1024,1024]{1,0:T(8,128)(2,1)S(1)} %copy-done.31, bf16[1024,1024]{1,0:T(8,128)(2,1)S(1)} %copy-done.32, ...), custom_call_target="tpu_custom_call" | custom-call | flops 16106127360 | bytes 32505856 | tf_op jit(solution)/shard_map/pallas_call | solution.py:547
  461.2 3.9 fusion.70
  466.4 27.6 %collective-permute-done.20.refs_2_ = bf16[1024,640]{1,0:T(8,128)(2,1)S(1)} collective-permute-done((bf16[1024,640]{1,0:T(8,128)(2,1)S(1)}, bf16[1024,640]{1,0:T(8,128)(2,1)S(1)}, u32[]{:S(2)}, u32[]{:S(2)}) %collective-permute-start.20) | collective-permute-done | bytes 1310752 | tf_op jit(solution)/shard_map/ppermute | solution.py:38
  496.9 11.4 %collective-permute-done.22.refs_4_ = bf16[512,640]{1,0:T(8,128)(2,1)S(1)} collective-permute-done((bf16[512,640]{1,0:T(8,128)(2,1)S(1)}, bf16[512,640]{1,0:T(8,128)(2,1)S(1)}, u32[]{:S(2)}, u32[]{:S(2)}) %collective-permute-start.22) | collective-permute-done | bytes 655392 | tf_op jit(solution)/shard_map/ppermute | solution.py:38
  509.4 6.9 shard_map.177
  516.3 8.0 shard_map.181
  524.3 3.7 collective-permute-done.42.right_ref
  529.5 3.6 shard_map.182
  533.1 3.0 copy-done.3
  536.1 6.8 shard_map.183
  546.0 12.5 %collective-permute-done.44.right_ref = bf16[1280,3072]{1,0:T(8,128)(2,1)S(1)} collective-permute-done((bf16[1280,3072]{1,0:T(8,128)(2,1)}, bf16[1280,3072]{1,0:T(8,128)(2,1)S(1)}, u32[]{:S(2)}, u32[]{:S(2)}) %collective-permute-start.44) | collective-permute-done | bytes 7864352 | tf_op jit(solution)/shard_map/ppermute | solution.py:785
  558.5 3.3 copy-done.2
  563.7 3.1 copy-done
  566.8 4.8 all-to-all-start.2
  571.7 17.1 %all-to-all-done.2 = bf16[4,256,640]{2,1,0:T(8,128)(2,1)} async-done(((bf16[4,256,640]{2,1,0:T(8,128)(2,1)}), bf16[4,256,640]{2,1,0:T(8,128)(2,1)}, u32[]{:S(2)}, u32[]{:S(2)}) %all-to-all-start.2) | async-done | bytes 1310752 | tf_op jit(solution)/shard_map/all_to_all | solution.py:144
  593.0 15.6 %att_b.1 = (bf16[256,2560]{1,0:T(8,128)(2,1)S(1)}, f32[1024,512]{1,0:T(8,128)S(1)}) custom-call(s32[1]{0:T(128)} %bitcast.1.first_ref, bf16[256,3072]{1,0:T(8,128)(2,1)S(1)} %bitcast.130, bf16[1024,512]{1,0:T(8,128)(2,1)S(1)} %copy-done.19, f32[256,128]{1,0:T(8,128)S(1)} %copy-done.27, f32[256,128]{1,0:T(8,128)S(1)} %copy-done.25, s32[256,1]{1,0:T(8,128)S(1)} %copy-done.21, ...), custom_call_target="tpu_custom_call" | custom-call | flops 6710886400 | bytes 8388608 | tf_op jit(solution)/shard_map/att_b/pallas_call | solution.py:433
  611.7 4.8 collective-permute-done.23
  618.7 3.7 collective-permute-done.24
  625.7 3.8 collective-permute-done.26
  633.7 4.3 all-to-all-start.3
  638.1 3.7 multiply_reduce_fusion
  641.9 13.5 %shard_map.175.refs_2_ = f32[1024,2560]{1,0:T(8,128)} custom-call(bf16[1024,896]{1,0:T(8,128)(2,1)S(1)} %get-tuple-element.81.hidden_ref.refs_0_, bf16[2560,2688]{1,0:T(8,128)(2,1)} %all-gather.3.cloned.1.call-done.refs_2_.refs_1_), custom_call_target="tpu_custom_call" | custom-call | flops 4697620480 | bytes 24248320 | tf_op jit(solution)/shard_map/pallas_call | solution.py:648
  655.3 14.1 %shard_map.176 = (bf16[2,512,640]{2,1,0:T(8,128)(2,1)}, bf16[2,512,640]{2,1,0:T(8,128)(2,1)}, bf16[2,512,640]{2,1,0:T(8,128)(2,1)S(1)}, bf16[2,512,640]{2,1,0:T(8,128)(2,1)S(1)}) custom-call(s32[1]{0:T(128)} %bitcast.me_ref, bf16[1024,1024]{1,0:T(8,128)(2,1)} %get-tuple-element.80.hidden_ref.refs_0_, ...), custom_call_target="tpu_custom_call" | custom-call | flops 5368709120 | bytes 23068672 | tf_op jit(solution)/shard_map/pallas_call | solution.py:689
  673.6 9.3 %shard_map.178 = (bf16[2,512,640]{2,1,0:T(8,128)(2,1)S(1)}, bf16[2,512,640]{2,1,0:T(8,128)(2,1)}, bf16[2,512,640]{2,1,0:T(8,128)(2,1)S(1)}, bf16[2,512,640]{2,1,0:T(8,128)(2,1)S(1)}) custom-call(s32[1]{0:T(128)} %bitcast.me_ref, bf16[1024,768]{1,0:T(8,128)(2,1)} %bitcast.35.refs_0_, bf16[2560,1408]{1,0:T(8,128)(2,1)} %get-tuple-element.60.refs_1_.refs_5_.refs_0_), custom_call_target="tpu_custom_call" | custom-call | flops 4026531840 | bytes 14024704 | tf_op jit(solution)/shard_map/pallas_call | solution.py:689
  687.2 9.2 %shard_map.179 = (bf16[1280,768]{1,0:T(8,128)(2,1)S(1)}, bf16[1280,768]{1,0:T(8,128)(2,1)}, f32[2560,1]{1,0:T(8,128)S(1)}) custom-call(s32[1]{0:T(128)} %bitcast.14.core_ref, bf16[1024,2560]{1,0:T(8,128)(2,1)} %get-tuple-element.91.left_ref, bf16[1024,768]{1,0:T(8,128)(2,1)S(1)} %multiply_convert_fusion.2.right_ref, ...), custom_call_target="tpu_custom_call" | custom-call | flops 4026531840 | bytes 10747904 | tf_op jit(solution)/shard_map/pallas_call | solution.py:514
  703.4 3.1 collective-permute-done.37
  710.4 7.2 collective-permute-done.38
  719.1 9.4 %collective-permute-done.28 = bf16[2,512,640]{2,1,0:T(8,128)(2,1)} collective-permute-done((bf16[2,512,640]{2,1,0:T(8,128)(2,1)}, bf16[2,512,640]{2,1,0:T(8,128)(2,1)}, u32[]{:S(2)}, u32[]{:S(2)}) %collective-permute-start.28) | collective-permute-done | bytes 1310752 | tf_op jit(solution)/shard_map/ppermute | solution.py:38
  730.6 7.3 collective-permute-done.39
  739.4 6.8 shard_map.180
  746.2 10.0 %collective-permute-done.35 = f32[4,256]{1,0:T(4,128)S(1)} collective-permute-done((f32[4,256]{1,0:T(4,128)S(1)}, f32[4,256]{1,0:T(4,128)S(1)}, u32[]{:S(2)}, u32[]{:S(2)}) %collective-permute-start.35) | collective-permute-done | bytes 4128 | tf_op jit(solution)/shard_map/ppermute | solution.py:38
  763.9 10.3 %collective-permute-done.27 = bf16[512,640]{1,0:T(8,128)(2,1)} collective-permute-done((bf16[512,640]{1,0:T(8,128)(2,1)}, bf16[512,640]{1,0:T(8,128)(2,1)}, u32[]{:S(2)}, u32[]{:S(2)}) %collective-permute-start.27) | collective-permute-done | bytes 655392 | tf_op jit(solution)/shard_map/ppermute | solution.py:38
  777.1 10.6 %collective-permute-done.33 = bf16[512,640]{1,0:T(8,128)(2,1)S(1)} collective-permute-done((bf16[512,640]{1,0:T(8,128)(2,1)S(1)}, bf16[512,640]{1,0:T(8,128)(2,1)S(1)}, u32[]{:S(2)}, u32[]{:S(2)}) %collective-permute-start.33) | collective-permute-done | bytes 655392 | tf_op jit(solution)/shard_map/ppermute | solution.py:38
  791.4 3.2 fusion.22
  796.5 3.2 fusion.74
  799.7 27.8 %reduce-scatter.11.cloned.1.call-done = bf16[320,3072]{1,0:T(8,128)(2,1)} async-done(((bf16[1280,3072]{1,0:T(8,128)(2,1)}), bf16[320,3072]{1,0:T(8,128)(2,1)}) %reduce-scatter.11.cloned.1.call-update) | async-done | bytes 1966096 | tf_op jit(solution)/shard_map/reduce_scatter | solution.py:788
  830.1 2.9 fusion.26
  834.5 37.8 %reduce-scatter.5.cloned.1.call-done = bf16[320,768]{1,0:T(8,128)(2,1)} async-done(((bf16[1280,768]{1,0:T(8,128)(2,1)}), bf16[320,768]{1,0:T(8,128)(2,1)}) %reduce-scatter.5.cloned.1.call-update) | async-done | bytes 491536 | tf_op jit(solution)/shard_map/reduce_scatter | solution.py:788
  (329 shorter events, 134.0 us)
Async XLA Ops:
  7.2 261.8 %all-gather.3.cloned.1.call-start = ((), (), s32[]{:S(2)}) async-start(), calls=%async_computation.8 | async-start | bytes 15482880 | tf_op jit(solution)/shard_map/all_gather | solution.py:780
  75.7 269.0 %all-gather.5.cloned.1.call-start = ((), (), s32[]{:S(2)}) async-start(), calls=%async_computation.9 | async-start | bytes 17694720 | tf_op jit(solution)/shard_map/all_gather | solution.py:780
  85.5 23.8 %all-to-all-start = ((bf16[4,256,768]{2,1,0:T(8,128)(2,1)}), bf16[4,256,768]{2,1,0:T(8,128)(2,1)S(1)}, u32[]{:S(2)}, u32[]{:S(2)}) async-start(bf16[4,256,768]{2,1,0:T(8,128)(2,1)} %bitcast.4), calls=%async_computation | async-start | bytes 3145728 | tf_op jit(solution)/shard_map/all_to_all | solution.py:144
  89.3 705.2 %reduce-scatter.7.cloned.1.call-start = ((), (), s32[]{:S(2)}) async-start(), calls=%async_computation.11 | async-start | bytes 2048000 | tf_op jit(solution)/shard_map/reduce_scatter | solution.py:788
  111.0 27.5 %copy-start.24 = (f32[256,128]{1,0:T(8,128)}, f32[256,128]{1,0:T(8,128)S(1)}, u32[]{:S(2)}) copy-start(f32[256,128]{1,0:T(8,128)S(1)} %get-tuple-element.144.sin_ref) | copy-start | bytes 393220
  111.9 7.9 collective-permute-start
  113.3 8.0 collective-permute-start.1
  119.8 5.0 collective-permute-start.2
  122.3 5.0 collective-permute-start.3
  165.2 27.2 %collective-permute-start.4 = (bf16[2,512,640]{2,1,0:T(8,128)(2,1)S(1)}, bf16[2,512,640]{2,1,0:T(8,128)(2,1)S(1)}, u32[]{:S(2)}, u32[]{:S(2)}) collective-permute-start(bf16[2,512,640]{2,1,0:T(8,128)(2,1)S(1)} %get-tuple-element.63), channel_id=1, source_target_pairs={{0,1},{1,0},{2,3},{3,2},{4,5},{5,4},{6,7},{7,6},{8,9},{9,8},{10,11... | collective-permute-start | bytes 3932168 | tf_op jit(solution)/shard_map/ppermute | solution.py:38
  166.1 28.7 %collective-permute-start.6 = (bf16[2,512,640]{2,1,0:T(8,128)(2,1)S(1)}, bf16[2,512,640]{2,1,0:T(8,128)(2,1)S(1)}, u32[]{:S(2)}, u32[]{:S(2)}) collective-permute-start(bf16[2,512,640]{2,1,0:T(8,128)(2,1)S(1)} %get-tuple-element.65), channel_id=1, source_target_pairs={{0,2},{1,3},{2,0},{3,1},{4,6},{5,7},{6,4},{7,5},{8,10},{9,11},{10,... | collective-permute-start | bytes 3932168 | tf_op jit(solution)/shard_map/ppermute | solution.py:38
  193.5 13.9 %collective-permute-start.5 = (bf16[512,640]{1,0:T(8,128)(2,1)}, bf16[512,640]{1,0:T(8,128)(2,1)S(1)}, u32[]{:S(2)}, u32[]{:S(2)}) collective-permute-start(bf16[512,640]{1,0:T(8,128)(2,1)} %fusion.34), channel_id=1, source_target_pairs={{0,2},{1,3},{2,0},{3,1},{4,6},{5,7},{6,4},{7,5},{8,10},{9,11},{10,... | collective-permute-start | bytes 1966088 | tf_op jit(solution)/shard_map/ppermute | solution.py:38
  196.9 12.8 %collective-permute-start.7 = (bf16[512,640]{1,0:T(8,128)(2,1)}, bf16[512,640]{1,0:T(8,128)(2,1)}, u32[]{:S(2)}, u32[]{:S(2)}) collective-permute-start(bf16[512,640]{1,0:T(8,128)(2,1)} %fusion.35), channel_id=1, source_target_pairs={{0,1},{1,0},{2,3},{3,2},{4,5},{5,4},{6,7},{7,6},{8,9},{9,8},{10,11... | collective-permute-start | bytes 1966088 | tf_op jit(solution)/shard_map/ppermute | solution.py:38
  216.4 26.0 %collective-permute-start.8 = (bf16[1024,640]{1,0:T(8,128)(2,1)S(1)}, bf16[1024,640]{1,0:T(8,128)(2,1)S(1)}, u32[]{:S(2)}, u32[]{:S(2)}) collective-permute-start(bf16[1024,640]{1,0:T(8,128)(2,1)S(1)} %get-tuple-element.112), channel_id=1, source_target_pairs={{0,1},{1,0},{2,3},{3,2},{4,5},{5,4},{6,7},{7,6},{8,9},{9,8},{10,11... | collective-permute-start | bytes 3932168 | tf_op jit(solution)/shard_map/ppermute | solution.py:38
  216.5 27.9 %collective-permute-start.9 = (bf16[1024,640]{1,0:T(8,128)(2,1)S(1)}, bf16[1024,640]{1,0:T(8,128)(2,1)S(1)}, u32[]{:S(2)}, u32[]{:S(2)}) collective-permute-start(bf16[1024,640]{1,0:T(8,128)(2,1)S(1)} %get-tuple-element.112), channel_id=1, source_target_pairs={{0,2},{1,3},{2,0},{3,1},{4,6},{5,7},{6,4},{7,5},{8,10},{9,11},{10,... | collective-permute-start | bytes 3932168 | tf_op jit(solution)/shard_map/ppermute | solution.py:38
  243.3 13.2 %collective-permute-start.10 = (bf16[512,640]{1,0:T(8,128)(2,1)}, bf16[512,640]{1,0:T(8,128)(2,1)S(1)}, u32[]{:S(2)}, u32[]{:S(2)}) collective-permute-start(bf16[512,640]{1,0:T(8,128)(2,1)} %slice.270), channel_id=1, source_target_pairs={{0,2},{1,3},{2,0},{3,1},{4,6},{5,7},{6,4},{7,5},{8,10},{9,11},{10,... | collective-permute-start | bytes 1966088 | tf_op jit(solution)/shard_map/ppermute | solution.py:38
  246.3 11.2 %collective-permute-start.11 = (bf16[512,640]{1,0:T(8,128)(2,1)}, bf16[512,640]{1,0:T(8,128)(2,1)}, u32[]{:S(2)}, u32[]{:S(2)}) collective-permute-start(bf16[512,640]{1,0:T(8,128)(2,1)} %slice.271), channel_id=1, source_target_pairs={{0,1},{1,0},{2,3},{3,2},{4,5},{5,4},{6,7},{7,6},{8,9},{9,8},{10,11... | collective-permute-start | bytes 1966088 | tf_op jit(solution)/shard_map/ppermute | solution.py:38
  377.3 55.9 %copy-start.32 = (bf16[1024,1024]{1,0:T(8,128)(2,1)S(1)}, bf16[1024,1024]{1,0:T(8,128)(2,1)}, u32[]{:S(2)}) copy-start(bf16[1024,1024]{1,0:T(8,128)(2,1)} %get-tuple-element.117.refs_1_.d_up_ref) | copy-start | bytes 6291460
  396.1 37.2 %copy-start.31 = (bf16[1024,1024]{1,0:T(8,128)(2,1)S(1)}, bf16[1024,1024]{1,0:T(8,128)(2,1)}, u32[]{:S(2)}) copy-start(bf16[1024,1024]{1,0:T(8,128)(2,1)} %get-tuple-element.113.refs_0_.d_gate_ref) | copy-start | bytes 6291460
  396.1 32.8 %collective-permute-start.14 = (bf16[2,512,640]{2,1,0:T(8,128)(2,1)S(1)}, bf16[2,512,640]{2,1,0:T(8,128)(2,1)S(1)}, u32[]{:S(2)}, u32[]{:S(2)}) collective-permute-start(bf16[2,512,640]{2,1,0:T(8,128)(2,1)S(1)} %get-tuple-element.75), channel_id=1, source_target_pairs={{0,2},{1,3},{2,0},{3,1},{4,6},{5,7},{6,4},{7,5},{8,10},{9,11},{10,... | collective-permute-start | bytes 3932168 | tf_op jit(solution)/shard_map/ppermute | solution.py:38
  397.6 33.0 %collective-permute-start.12 = (bf16[2,512,640]{2,1,0:T(8,128)(2,1)S(1)}, bf16[2,512,640]{2,1,0:T(8,128)(2,1)S(1)}, u32[]{:S(2)}, u32[]{:S(2)}) collective-permute-start(bf16[2,512,640]{2,1,0:T(8,128)(2,1)S(1)} %get-tuple-element.73), channel_id=1, source_target_pairs={{0,1},{1,0},{2,3},{3,2},{4,5},{5,4},{6,7},{7,6},{8,9},{9,8},{10,11... | collective-permute-start | bytes 3932168 | tf_op jit(solution)/shard_map/ppermute | solution.py:38
  399.1 29.3 %collective-permute-start.16 = (f32[8,128]{1,0:T(8,128)S(1)}, f32[8,128]{1,0:T(8,128)S(1)}, u32[]{:S(2)}, u32[]{:S(2)}) collective-permute-start(f32[8,128]{1,0:T(8,128)S(1)} %add_bitcast_fusion), channel_id=1, source_target_pairs={{0,1},{1,0},{2,3},{3,2},{4,5},{5,4},{6,7},{7,6},{8,9},{9,8},{10,11... | collective-permute-start | bytes 12296 | tf_op jit(solution)/shard_map/ppermute | solution.py:38
  428.4 29.8 %collective-permute-start.17 = (f32[8,128]{1,0:T(8,128)S(1)}, f32[8,128]{1,0:T(8,128)S(1)}, u32[]{:S(2)}, u32[]{:S(2)}) collective-permute-start(f32[8,128]{1,0:T(8,128)S(1)} %fusion.82), channel_id=1, source_target_pairs={{0,2},{1,3},{2,0},{3,1},{4,6},{5,7},{6,4},{7,5},{8,10},{9,11},{10,... | collective-permute-start | bytes 12296 | tf_op jit(solution)/shard_map/ppermute | solution.py:38
  429.1 29.2 %collective-permute-start.15 = (bf16[512,640]{1,0:T(8,128)(2,1)S(1)}, bf16[512,640]{1,0:T(8,128)(2,1)S(1)}, u32[]{:S(2)}, u32[]{:S(2)}) collective-permute-start(bf16[512,640]{1,0:T(8,128)(2,1)S(1)} %fusion.37), channel_id=1, source_target_pairs={{0,1},{1,0},{2,3},{3,2},{4,5},{5,4},{6,7},{7,6},{8,9},{9,8},{10,11... | collective-permute-start | bytes 1966088 | tf_op jit(solution)/shard_map/ppermute | solution.py:38
  430.6 27.6 %copy-start.54 = (bf16[2,512,640]{2,1,0:T(8,128)(2,1)}, bf16[2,512,640]{2,1,0:T(8,128)(2,1)S(1)}, u32[]{:S(2)}) copy-start(bf16[2,512,640]{2,1,0:T(8,128)(2,1)S(1)} %collective-permute-done.12) | copy-start | bytes 3932164
  431.8 26.7 %collective-permute-start.13 = (bf16[512,640]{1,0:T(8,128)(2,1)}, bf16[512,640]{1,0:T(8,128)(2,1)}, u32[]{:S(2)}, u32[]{:S(2)}) collective-permute-start(bf16[512,640]{1,0:T(8,128)(2,1)} %fusion.36), channel_id=1, source_target_pairs={{0,2},{1,3},{2,0},{3,1},{4,6},{5,7},{6,4},{7,5},{8,10},{9,11},{10,... | collective-permute-start | bytes 1966088 | tf_op jit(solution)/shard_map/ppermute | solution.py:38
  459.6 49.8 %slice-start = ((s8[7208960]{0:T(1024)(128)(4,1)}), s8[4194304]{0:T(1024)(128)(4,1)S(1)}, s32[]{:S(2)}) async-start(s8[7208960]{0:T(1024)(128)(4,1)} %bitcast.126), calls=%async_computation.14 | async-start | bytes 8388608
  461.1 48.2 %slice-start.1 = ((s8[7208960]{0:T(1024)(128)(4,1)}), s8[3014656]{0:T(1024)(128)(4,1)S(1)}, s32[]{:S(2)}) async-start(s8[7208960]{0:T(1024)(128)(4,1)} %bitcast.126), calls=%async_computation.15 | async-start | bytes 6029312
  465.1 28.9 %collective-permute-start.20 = (bf16[1024,640]{1,0:T(8,128)(2,1)S(1)}, bf16[1024,640]{1,0:T(8,128)(2,1)S(1)}, u32[]{:S(2)}, u32[]{:S(2)}) collective-permute-start(bf16[1024,640]{1,0:T(8,128)(2,1)S(1)} %get-tuple-element.79.refs_0_), channel_id=1, source_target_pairs={{0,2},{1,3},{2,0},{3,1},{4,6},{5,7},{6,4},{7,5},{8,10},{9,11},{10,... | collective-permute-start | bytes 3932168 | tf_op jit(solution)/shard_map/ppermute | solution.py:38
  465.6 29.6 %collective-permute-start.19 = (bf16[1024,640]{1,0:T(8,128)(2,1)S(1)}, bf16[1024,640]{1,0:T(8,128)(2,1)S(1)}, u32[]{:S(2)}, u32[]{:S(2)}) collective-permute-start(bf16[1024,640]{1,0:T(8,128)(2,1)S(1)} %get-tuple-element.79.refs_0_), channel_id=1, source_target_pairs={{0,1},{1,0},{2,3},{3,2},{4,5},{5,4},{6,7},{7,6},{8,9},{9,8},{10,11... | collective-permute-start | bytes 3932168 | tf_op jit(solution)/shard_map/ppermute | solution.py:38
  466.4 66.7 %collective-permute-start.43 = (bf16[1280,2688]{1,0:T(8,128)(2,1)}, bf16[1280,2688]{1,0:T(8,128)(2,1)}, u32[]{:S(2)}, u32[]{:S(2)}) collective-permute-start(bf16[1280,2688]{1,0:T(8,128)(2,1)} %get-tuple-element.105), channel_id=1, source_target_pairs={{0,4},{4,0},{8,12},{12,8},{16,20},{20,16},{24,28},{28,24},{1,5},{5... | collective-permute-start | bytes 20643848 | tf_op jit(solution)/shard_map/ppermute | solution.py:785
  494.1 14.3 %collective-permute-start.22 = (bf16[512,640]{1,0:T(8,128)(2,1)S(1)}, bf16[512,640]{1,0:T(8,128)(2,1)S(1)}, u32[]{:S(2)}, u32[]{:S(2)}) collective-permute-start(bf16[512,640]{1,0:T(8,128)(2,1)S(1)} %slice.285), channel_id=1, source_target_pairs={{0,1},{1,0},{2,3},{3,2},{4,5},{5,4},{6,7},{7,6},{8,9},{9,8},{10,11... | collective-permute-start | bytes 1966088 | tf_op jit(solution)/shard_map/ppermute | solution.py:38
  495.3 14.1 %collective-permute-start.21 = (bf16[512,640]{1,0:T(8,128)(2,1)S(1)}, bf16[512,640]{1,0:T(8,128)(2,1)S(1)}, u32[]{:S(2)}, u32[]{:S(2)}) collective-permute-start(bf16[512,640]{1,0:T(8,128)(2,1)S(1)} %slice.284), channel_id=1, source_target_pairs={{0,2},{1,3},{2,0},{3,1},{4,6},{5,7},{6,4},{7,5},{8,10},{9,11},{10,... | collective-permute-start | bytes 1966088 | tf_op jit(solution)/shard_map/ppermute | solution.py:38
  524.3 3.7 collective-permute-start.42
  533.1 263.4 %reduce-scatter.9.cloned.1.call-start = ((), (), s32[]{:S(2)}) async-start(), calls=%async_computation.12 | async-start | bytes 8601600 | tf_op jit(solution)/shard_map/reduce_scatter | solution.py:788
  545.8 281.7 %reduce-scatter.11.cloned.1.call-start = ((), (), s32[]{:S(2)}) async-start(), calls=%async_computation.13 | async-start | bytes 9830400 | tf_op jit(solution)/shard_map/reduce_scatter | solution.py:788
  545.8 12.7 %collective-permute-start.44 = (bf16[1280,3072]{1,0:T(8,128)(2,1)}, bf16[1280,3072]{1,0:T(8,128)(2,1)S(1)}, u32[]{:S(2)}, u32[]{:S(2)}) collective-permute-start(bf16[1280,3072]{1,0:T(8,128)(2,1)} %get-tuple-element.106), channel_id=1, source_target_pairs={{0,4},{4,0},{8,12},{12,8},{16,20},{20,16},{24,28},{28,24},{1,5},{5... | collective-permute-start | bytes 23592968 | tf_op jit(solution)/shard_map/ppermute | solution.py:785
  566.8 21.9 %all-to-all-start.2 = ((bf16[4,256,640]{2,1,0:T(8,128)(2,1)}), bf16[4,256,640]{2,1,0:T(8,128)(2,1)}, u32[]{:S(2)}, u32[]{:S(2)}) async-start(bf16[4,256,640]{2,1,0:T(8,128)(2,1)} %bitcast.24), calls=%async_computation.2 | async-start | bytes 2621440 | tf_op jit(solution)/shard_map/all_to_all | solution.py:144
  608.9 7.6 collective-permute-start.23
  611.2 7.5 collective-permute-start.25
  617.2 5.2 collective-permute-start.24
  624.2 5.2 collective-permute-start.26
  633.7 39.8 %all-to-all-start.3 = ((bf16[256,4,768]{2,0,1:T(8,128)(2,1)}), bf16[256,4,768]{2,0,1:T(8,128)(2,1)}, u32[]{:S(2)}, u32[]{:S(2)}) async-start(bf16[256,4,768]{2,0,1:T(8,128)(2,1)} %bitcast.124), calls=%async_computation.3 | async-start | bytes 3145728 | tf_op jit(solution)/shard_map/all_to_all | solution.py:148
  638.1 234.2 %reduce-scatter.5.cloned.1.call-start = ((), (), s32[]{:S(2)}) async-start(), calls=%async_computation.10 | async-start | bytes 2457600 | tf_op jit(solution)/shard_map/reduce_scatter | solution.py:788
  671.6 30.8 %collective-permute-start.18 = (bf16[2,512,640]{2,1,0:T(8,128)(2,1)}, bf16[2,512,640]{2,1,0:T(8,128)(2,1)}, u32[]{:S(2)}, u32[]{:S(2)}) collective-permute-start(bf16[2,512,640]{2,1,0:T(8,128)(2,1)} %get-tuple-element.83), channel_id=1, source_target_pairs={{0,1},{1,0},{2,3},{3,2},{4,5},{5,4},{6,7},{7,6},{8,9},{9,8},{10,11... | collective-permute-start | bytes 3932168 | tf_op jit(solution)/shard_map/ppermute | solution.py:38
  696.4 42.9 %collective-permute-start.41 = (bf16[1280,768]{1,0:T(8,128)(2,1)}, bf16[1280,768]{1,0:T(8,128)(2,1)}, u32[]{:S(2)}, u32[]{:S(2)}) collective-permute-start(bf16[1280,768]{1,0:T(8,128)(2,1)} %get-tuple-element.100), channel_id=1, source_target_pairs={{0,4},{4,0},{8,12},{12,8},{16,20},{20,16},{24,28},{28,24},{1,5},{5... | collective-permute-start | bytes 5898248 | tf_op jit(solution)/shard_map/ppermute | solution.py:785
  696.4 32.0 %collective-permute-start.28 = (bf16[2,512,640]{2,1,0:T(8,128)(2,1)}, bf16[2,512,640]{2,1,0:T(8,128)(2,1)}, u32[]{:S(2)}, u32[]{:S(2)}) collective-permute-start(bf16[2,512,640]{2,1,0:T(8,128)(2,1)} %get-tuple-element.89), channel_id=1, source_target_pairs={{0,2},{1,3},{2,0},{3,1},{4,6},{5,7},{6,4},{7,5},{8,10},{9,11},{10,... | collective-permute-start | bytes 3932168 | tf_op jit(solution)/shard_map/ppermute | solution.py:38
  698.5 30.0 %copy-start.10 = (bf16[2,512,640]{2,1,0:T(8,128)(2,1)S(1)}, bf16[2,512,640]{2,1,0:T(8,128)(2,1)}, u32[]{:S(2)}) copy-start(bf16[2,512,640]{2,1,0:T(8,128)(2,1)} %copy-done.9) | copy-start | bytes 3932164
  698.5 3.8 collective-permute-start.36
  701.1 57.9 %collective-permute-start.32 = (bf16[2,512,640]{2,1,0:T(8,128)(2,1)}, bf16[2,512,640]{2,1,0:T(8,128)(2,1)}, u32[]{:S(2)}, u32[]{:S(2)}) collective-permute-start(bf16[2,512,640]{2,1,0:T(8,128)(2,1)} %get-tuple-element.95), channel_id=1, source_target_pairs={{0,2},{1,3},{2,0},{3,1},{4,6},{5,7},{6,4},{7,5},{8,10},{9,11},{10,... | collective-permute-start | bytes 3932168 | tf_op jit(solution)/shard_map/ppermute | solution.py:38
  702.3 4.2 collective-permute-start.37
  702.4 7.9 collective-permute-start.34
  706.5 55.4 %collective-permute-start.30 = (bf16[2,512,640]{2,1,0:T(8,128)(2,1)}, bf16[2,512,640]{2,1,0:T(8,128)(2,1)}, u32[]{:S(2)}, u32[]{:S(2)}) collective-permute-start(bf16[2,512,640]{2,1,0:T(8,128)(2,1)} %copy-done.28), channel_id=1, source_target_pairs={{0,1},{1,0},{2,3},{3,2},{4,5},{5,4},{6,7},{7,6},{8,9},{9,8},{10,11... | collective-permute-start | bytes 3932168 | tf_op jit(solution)/shard_map/ppermute | solution.py:38
  710.2 7.3 collective-permute-start.38
  717.6 38.6 %collective-permute-start.35 = (f32[4,256]{1,0:T(4,128)S(1)}, f32[4,256]{1,0:T(4,128)S(1)}, u32[]{:S(2)}, u32[]{:S(2)}) collective-permute-start(f32[4,256]{1,0:T(4,128)S(1)} %add.420), channel_id=1, source_target_pairs={{0,2},{1,3},{2,0},{3,1},{4,6},{5,7},{6,4},{7,5},{8,10},{9,11},{10,... | collective-permute-start | bytes 12296 | tf_op jit(solution)/shard_map/ppermute | solution.py:38
  728.5 9.4 %collective-permute-start.39 = (f32[8,320]{1,0:T(8,128)S(1)}, f32[8,320]{1,0:T(8,128)S(1)}, u32[]{:S(2)}, u32[]{:S(2)}) collective-permute-start(f32[8,320]{1,0:T(8,128)S(1)} %add.425), channel_id=1, source_target_pairs={{0,1},{1,0},{2,3},{3,2},{4,5},{5,4},{6,7},{7,6},{8,9},{9,8},{10,11... | collective-permute-start | bytes 30728 | tf_op jit(solution)/shard_map/ppermute | solution.py:38
  737.9 20.4 %collective-permute-start.40 = (f32[8,320]{1,0:T(8,128)S(1)}, f32[8,320]{1,0:T(8,128)S(1)}, u32[]{:S(2)}, u32[]{:S(2)}) collective-permute-start(f32[8,320]{1,0:T(8,128)S(1)} %add.426), channel_id=1, source_target_pairs={{0,2},{1,3},{2,0},{3,1},{4,6},{5,7},{6,4},{7,5},{8,10},{9,11},{10,... | collective-permute-start | bytes 30728 | tf_op jit(solution)/shard_map/ppermute | solution.py:38
  756.2 17.9 %collective-permute-start.27 = (bf16[512,640]{1,0:T(8,128)(2,1)}, bf16[512,640]{1,0:T(8,128)(2,1)}, u32[]{:S(2)}, u32[]{:S(2)}) collective-permute-start(bf16[512,640]{1,0:T(8,128)(2,1)} %fusion.38), channel_id=1, source_target_pairs={{0,2},{1,3},{2,0},{3,1},{4,6},{5,7},{6,4},{7,5},{8,10},{9,11},{10,... | collective-permute-start | bytes 1966088 | tf_op jit(solution)/shard_map/ppermute | solution.py:38
  757.7 18.0 %collective-permute-start.29 = (bf16[512,640]{1,0:T(8,128)(2,1)}, bf16[512,640]{1,0:T(8,128)(2,1)S(1)}, u32[]{:S(2)}, u32[]{:S(2)}) collective-permute-start(bf16[512,640]{1,0:T(8,128)(2,1)} %fusion.39), channel_id=1, source_target_pairs={{0,1},{1,0},{2,3},{3,2},{4,5},{5,4},{6,7},{7,6},{8,9},{9,8},{10,11... | collective-permute-start | bytes 1966088 | tf_op jit(solution)/shard_map/ppermute | solution.py:38
  760.4 27.3 %collective-permute-start.33 = (bf16[512,640]{1,0:T(8,128)(2,1)S(1)}, bf16[512,640]{1,0:T(8,128)(2,1)S(1)}, u32[]{:S(2)}, u32[]{:S(2)}) collective-permute-start(bf16[512,640]{1,0:T(8,128)(2,1)S(1)} %fusion.41), channel_id=1, source_target_pairs={{0,1},{1,0},{2,3},{3,2},{4,5},{5,4},{6,7},{7,6},{8,9},{9,8},{10,11... | collective-permute-start | bytes 1966088 | tf_op jit(solution)/shard_map/ppermute | solution.py:38
  763.2 26.1 %collective-permute-start.31 = (bf16[512,640]{1,0:T(8,128)(2,1)S(1)}, bf16[512,640]{1,0:T(8,128)(2,1)S(1)}, u32[]{:S(2)}, u32[]{:S(2)}) collective-permute-start(bf16[512,640]{1,0:T(8,128)(2,1)S(1)} %fusion.40), channel_id=1, source_target_pairs={{0,2},{1,3},{2,0},{3,1},{4,6},{5,7},{6,4},{7,5},{8,10},{9,11},{10,... | collective-permute-start | bytes 1966088 | tf_op jit(solution)/shard_map/ppermute | solution.py:38
  799.7 29.9 %copy-start.47 = (bf16[320,1920]{1,0:T(8,128)(2,1)S(1)}, bf16[320,1920]{1,0:T(8,128)(2,1)}, u32[]{:S(2)}) copy-start(bf16[320,1920]{1,0:T(8,128)(2,1)} %refs_1_.1) | copy-start | bytes 3686404
  833.0 41.4 %collective-permute-start.45 = (f32[320]{0:T(512)S(1)}, f32[320]{0:T(512)S(1)}, u32[]{:S(2)}, u32[]{:S(2)}) collective-permute-start(f32[320]{0:T(512)S(1)} %get-tuple-element.122), channel_id=1, source_target_pairs={{0,1},{1,0},{2,3},{3,2},{4,5},{5,4},{6,7},{7,6},{8,9},{9,8},{10,11... | collective-permute-start | bytes 3848 | tf_op jit(solution)/shard_map/ppermute | solution.py:38
  874.4 4.3 collective-permute-start.46
  (67 other events, 564.7 us)
Sparse Core Ops, SparseCore 0:
  75.8 126.5 all-gather.2
  204.0 140.6 all-gather.4
  533.2 33.2 reduce-scatter.6
  568.7 119.2 reduce-scatter.8
  690.1 137.3 reduce-scatter.10
  830.2 42.0 reduce-scatter.4

commit v13 on v12

--- a/solution.py
+++ b/solution.py
@@ -177,7 +177,12 @@
     def cols(block):
         return pl.ds(pl.multiple_of(block * width, 128), width)
 
-    windows = (pl.ds(split, all_cols - split), pl.ds(0, split))
+    near_cols = split // 256 * 128
+    windows = (
+        pl.ds(split, all_cols - split),
+        pl.ds(0, near_cols),
+        pl.ds(near_cols, split - near_cols),
+    )
 
     def block(index, part):
         return weight_ref.at[pl.ds(pl.multiple_of(index * shard, 16), shard), windows[part]]
@@ -196,7 +201,7 @@
     to_x, to_y = x_copy(x_ref, mine, 0, 1), x_copy(x_ref, mine, 1, 2)
     keeps = [pltpu.make_async_copy(x_ref, mine, own.at[0])]
     loads = [
-        pltpu.make_async_copy(weight, to, own.at[3 + at])
+        pltpu.make_async_copy(weight, to, own.at[4 + at])
         for at, (weight, to) in enumerate(zip(weights, held))
     ]
 
@@ -230,7 +235,8 @@
                 value = (value.astype(F32) * gain).astype(BF16)
             out[:, at * count : (at + 1) * count] = value
         if start == 0:
-            send_own(left_ref, 1)
+            for part in (1, 2):
+                send_own(left_ref.at[:, windows[part]], part)
 
     def relay(distance, part):
         low, high = tok - 2 * distance, tok + 2 * distance
@@ -257,10 +263,10 @@
 
             w_copy(source, high, part, w_core.at[high, part], tok ^ 1).start()
 
-    relay(1, 0)
-    relay(1, 1)
+    for part in range(3):
+        relay(1, part)
     stores = [
-        pltpu.make_async_copy(out, to, own.at[7 + at])
+        pltpu.make_async_copy(out, to, own.at[8 + at])
         for at, (out, to) in enumerate(zip(joined, locals_ref))
     ]
     for copy in stores:
@@ -273,8 +279,8 @@
     to_y.wait_recv()
     bottom.start()
     for distance in range(2, pairs):
-        relay(distance, 0)
-        relay(distance, 1)
+        for part in range(3):
+            relay(distance, part)
     for copy in (*keeps, *stores):
         copy.wait()
     for copy in (top, bottom):
@@ -283,7 +289,7 @@
         copy.wait_send()
 
     for distance in range(pairs):
-        for part in range(2):
+        for part in range(3):
             mine = block(tok, part)
 
             @pl.when((level >= distance) & above)
@@ -316,8 +322,8 @@
         scratch_shapes=[pltpu.VMEM(array.shape, BF16) for array in weights]
         + [pltpu.VMEM(shape, BF16) for shape in (*locals_ff, weights[0].shape)]
         + [
-            dma((9,)), dma((4,)), dma((4,)), dma((pairs, 2)), dma((pairs, 2)),
-            dma((2 * pairs, 2)), dma((2 * pairs, 2)),
+            dma((10,)), dma((4,)), dma((4,)), dma((pairs, 3)), dma((pairs, 3)),
+            dma((2 * pairs, 3)), dma((2 * pairs, 3)),
         ],
         compiler_params=pltpu.CompilerParams(
             collective_id=0, has_side_effects=True, vmem_limit_bytes=60 << 20

time: 894 us -> 894 us (level)
  transfers between devices with their start and end apart: 56 -> 56, of which waited for: 30 -> 31; matrix products, arithmetic and copies ran while one was open for 13% -> 13% of each run, Pallas kernels for 20% -> 20%
where the time goes in v13:
time: 894 us; the launch traced here: 886 us
  waiting for transfers between devices  342 us (38%)
  Pallas kernels  264 us (30%)
  other arithmetic  69 us (8%)
  matrix products  68.5 us (8%)
  starting transfers between devices  59 us (7%)
  local copies, waits for them, and re-layouts  49.8 us (6%)
  blocking collectives  18.6 us (2%)
  between operations  15.3 us (2%)
    ppermute x40, waiting for transfers between devices, swap(): return lax.ppermute(block, 'mdl', [(i, i ^ distance) for i in range(size)])  204 us
    dot_general x7, matrix products, nn(): return jnp.dot(left_op, right_op, preferred_element_type=F32)  68.5 us
    pallas_call x1, Pallas kernels, first_gather(): pl.pallas_call(functools.partial(first_kernel, parts), out_shape=[jax.Sha...  66.8 us
    reduce_scatter x4, waiting for transfers between devices, pair_to_tok(): lax.psum_scatter(both, 'tok', scatter_dimension=0, tiled=True, axis_index...  65.6 us
    pallas_call x4, Pallas kernels, scatter_product(): pl.pallas_call(functools.partial(payload_kernel, starts), grid_spec=pltpu...  50 us
    pallas_call x2, Pallas kernels, part_grad(): pl.pallas_call(part_kernel, grid=(pairs,), out_shape=(out, out), in_specs...  48.5 us
    ppermute x40, starting transfers between devices, swap(): return lax.ppermute(block, 'mdl', [(i, i ^ distance) for i in range(size)])  45.4 us
    all_to_all x2, waiting for transfers between devices, rows_to_cols(): return lax.all_to_all(block, 'mdl', split_axis=0, concat_axis=1, tiled=True)  35.3 us
  transfers between devices with their start and end apart: 56, of which 31 were waited for; matrix products, arithmetic and copies ran while one was open for 13% of the time, Pallas kernels for 20%

profile of v13, /device:TPU:0, one launch (start us, length us, event | category | flops | bytes accessed | tf_op | source)
XLA Modules:
  0.0 886.3 jit_solution(9638491027087916202)
XLA Ops:
  8.7 66.8 %shard_map.169 = (bf16[1024,2560]{1,0:T(8,128)(2,1)}, bf16[2560,1408]{1,0:T(8,128)(2,1)}, bf16[320,2688]{1,0:T(8,128)(2,1)}, bf16[320,3072]{1,0:T(8,128)(2,1)}) custom-call(bf16[1024,640]{1,0:T(8,128)(2,1)} %x_ref.1, bf16[320,128]{1,0:T(8,128)(2,1)} %broadcast_select_fusion.gains_ref, bf16[320,640]{1,0:T(8,128)(2,1)} %bitcast.142, bf16[320,768]{1,0:T(8,128)(2,1)} %refs_0_.1, ...), custom_call_target="tpu_custom_call" | custom-call | tf_op jit(solution)/shard_map/pallas_call | solution.py:316
  76.3 9.0 %fusion.30 = bf16[1024,768]{1,0:T(8,128)(2,1)} fusion(bf16[1024,2560]{1,0:T(8,128)(2,1)} %get-tuple-element.91.left_ref, bf16[2560,1408]{1,0:T(8,128)(2,1)} %get-tuple-element.60.refs_1_.refs_5_.refs_0_), kind=kOutput, calls=%fused_computation.57 | convolution fusion | flops 4027318272 | bytes 10747904 | tf_op jit(solution)/shard_map/dot_general | solution.py:33
  85.4 3.8 all-to-all-start
  90.9 18.2 %all-to-all-done = bf16[4,256,768]{2,1,0:T(8,128)(2,1)S(1)} async-done(((bf16[4,256,768]{2,1,0:T(8,128)(2,1)}), bf16[4,256,768]{2,1,0:T(8,128)(2,1)S(1)}, u32[]{:S(2)}, u32[]{:S(2)}) %all-to-all-start) | async-done | bytes 1572896 | tf_op jit(solution)/shard_map/all_to_all | solution.py:144
  114.1 5.6 collective-permute-done
  127.2 11.2 %att_f.1 = (bf16[256,2560]{1,0:T(8,128)(2,1)S(1)}, f32[10,256,1]{2,1,0:T(8,128)S(1)}) custom-call(s32[1]{0:T(128)} %bitcast.1.first_ref, bf16[256,3072]{1,0:T(8,128)(2,1)S(1)} %bitcast.129, bf16[1024,512]{1,0:T(8,128)(2,1)S(1)} %constant_dynamic-update-slice_fusion.4.kv_ref, f32[256,128]{1,0:T(8,128)S(1)} %get-tuple-element.145.cos_ref, ...), custom_call_target="tpu_custom_call" | custom-call | flops 2684354560 | bytes 3670016 | tf_op jit(solution)/shard_map/att_f/pallas_call | solution.py:413
  138.6 18.6 %all_to_all.76 = bf16[256,4,640]{2,0,1:T(8,128)(2,1)} all-to-all(bf16[256,4,640]{2,0,1:T(8,128)(2,1)S(1)} %bitcast.138), channel_id=1, replica_groups=mesh['tok'=8,'mdl'=4] {'mdl'}, dimensions={1} | all-to-all | bytes 2621440 | tf_op jit(solution)/shard_map/all_to_all | solution.py:148
  157.1 7.9 shard_map.170
  166.5 25.7 %collective-permute-done.4 = bf16[2,512,640]{2,1,0:T(8,128)(2,1)S(1)} collective-permute-done((bf16[2,512,640]{2,1,0:T(8,128)(2,1)S(1)}, bf16[2,512,640]{2,1,0:T(8,128)(2,1)S(1)}, u32[]{:S(2)}, u32[]{:S(2)}) %collective-permute-start.4) | collective-permute-done | bytes 1310752 | tf_op jit(solution)/shard_map/ppermute | solution.py:38
  197.2 10.1 %collective-permute-done.5 = bf16[512,640]{1,0:T(8,128)(2,1)S(1)} collective-permute-done((bf16[512,640]{1,0:T(8,128)(2,1)}, bf16[512,640]{1,0:T(8,128)(2,1)S(1)}, u32[]{:S(2)}, u32[]{:S(2)}) %collective-permute-start.5) | collective-permute-done | bytes 655392 | tf_op jit(solution)/shard_map/ppermute | solution.py:38
  211.0 3.5 broadcast_in_dim.43
  217.9 24.4 %collective-permute-done.8 = bf16[1024,640]{1,0:T(8,128)(2,1)S(1)} collective-permute-done((bf16[1024,640]{1,0:T(8,128)(2,1)S(1)}, bf16[1024,640]{1,0:T(8,128)(2,1)S(1)}, u32[]{:S(2)}, u32[]{:S(2)}) %collective-permute-start.8) | collective-permute-done | bytes 1310752 | tf_op jit(solution)/shard_map/ppermute | solution.py:38
  251.7 4.7 collective-permute-done.10
  259.5 3.6 fusion
  263.2 5.8 fusion.1.rows_ref
  268.9 9.7 %fusion.12 = f32[896,1024]{0,1:T(8,128)S(1)} fusion(bf16[1024,2560]{1,0:T(8,128)(2,1)} %above_ref.2, bf16[2560,2688]{1,0:T(8,128)(2,1)} %all-gather.3.cloned.1.call-done.refs_2_.refs_1_), kind=kOutput, calls=%fused_computation.15 | convolution fusion | flops 4697620480 | bytes 13500416 | tf_op jit(solution)/shard_map/dot_general | solution.py:33
  278.6 7.9 fusion.8
  286.5 9.3 %add_reduce_fusion.1 = (f32[1024]{0:T(1024)S(1)}, bf16[1024,896]{1,0:T(8,128)(2,1)S(1)}, bf16[1024,896]{1,0:T(8,128)(2,1)S(1)}, bf16[1024,896]{1,0:T(8,128)(2,1)S(1)}) fusion(f32[1024,896]{1,0:T(8,128)S(1)} %fusion.8, f32[896,1024]{0,1:T(8,128)S(1)} %fusion.12, bf16[1024,2560]{1,0:T(8,128)(2,1)S(1)} %copy-done.46, ...), kind=kOutput, calls=%fused_computation.29 | convolution fusion | flops 4723309568 | bytes 22679552 | tf_op jit(solution)/shard_map/dot_general | solution.py:33
  295.8 23.6 %shard_map.171 = (bf16[1280,2688]{1,0:T(8,128)(2,1)}, bf16[1280,2688]{1,0:T(8,128)(2,1)}) custom-call(s32[1]{0:T(128)} %bitcast.14.core_ref, bf16[1024,2560]{1,0:T(8,128)(2,1)} %fusion.1.rows_ref, bf16[1024,2560]{1,0:T(8,128)(2,1)} %above_ref.2, bf16[1024,896]{1,0:T(8,128)(2,1)S(1)} %get-tuple-element.71.d_gate_ref.refs_0_, ...), custom_call_target="tpu_custom_call" | custom-call | flops 14092861440 | bytes 29753344 | tf_op jit(solution)/shard_map/pallas_call | solution.py:553
  319.4 15.3 %shard_map.172.refs_3_ = f32[1024,2560]{1,0:T(8,128)} custom-call(bf16[1024,896]{1,0:T(8,128)(2,1)S(1)} %get-tuple-element.71.d_gate_ref.refs_0_, bf16[1024,896]{1,0:T(8,128)(2,1)S(1)} %get-tuple-element.119.d_up_ref.refs_1_, bf16[2560,2688]{1,0:T(8,128)(2,1)} %all-gather.3.cloned.1.call-done.refs_2_.refs_1_), custom_call_target="tpu_custom_call" | custom-call | flops 9395240960 | bytes 24248320 | tf_op jit(solution)/shard_map/pallas_call | solution.py:654
  334.7 9.9 %all-gather.5.cloned.1.call-done.refs_2_.refs_1_ = bf16[2560,3072]{1,0:T(8,128)(2,1)} async-done(((bf16[320,3072]{1,0:T(8,128)(2,1)}), bf16[2560,3072]{1,0:T(8,128)(2,1)}) %all-gather.5.cloned.1.call-update) | async-done | bytes 15728656 | tf_op jit(solution)/shard_map/all_gather | solution.py:786
  344.6 10.7 %fusion.2 = f32[1024,1024]{1,0:T(8,128)} fusion(bf16[1024,2560]{1,0:T(8,128)(2,1)} %above_ref.2, bf16[2560,3072]{1,0:T(8,128)(2,1)} %all-gather.5.cloned.1.call-done.refs_2_.refs_1_), kind=kOutput, calls=%fused_computation.5 | convolution fusion | flops 5368709120 | bytes 14680064 | tf_op jit(solution)/shard_map/dot_general | solution.py:33
  355.3 8.9 %fusion.4 = f32[1024,1024]{1,0:T(8,128)} fusion(bf16[1024,2560]{1,0:T(8,128)(2,1)} %fusion.1.rows_ref, bf16[2560,3072]{1,0:T(8,128)(2,1)S(1)} %copy-done.42), kind=kOutput, calls=%fused_computation.7 | convolution fusion | flops 5368709120 | bytes 14680064 | tf_op jit(solution)/shard_map/dot_general | solution.py:33
  364.2 13.0 %fusion.67 = (bf16[1024,1024]{1,0:T(8,128)(2,1)}, f32[1024]{0:T(1024)S(1)}, bf16[1024,1024]{1,0:T(8,128)(2,1)}, bf16[1024,1024]{1,0:T(8,128)(2,1)}) fusion(f32[1024,1024]{1,0:T(8,128)} %fusion.2, f32[1024,1024]{1,0:T(8,128)} %fusion.4, bf16[1024,2560]{1,0:T(8,128)(2,1)S(1)} %bitcast.137, bf16[2560,3072]{1,0:T(8,128)(2,1)S(1)} %copy-done.42), kind=kOutput, calls=%fused_computation.158 | convolution fusion | flops 5398068224 | bytes 25169920 | tf_op jit(solution)/shard_map/dot_general | solution.py:33
  377.2 18.7 %shard_map.173 = (bf16[2,512,640]{2,1,0:T(8,128)(2,1)S(1)}, bf16[2,512,640]{2,1,0:T(8,128)(2,1)S(1)}, bf16[2,512,640]{2,1,0:T(8,128)(2,1)S(1)}, bf16[2,512,640]{2,1,0:T(8,128)(2,1)S(1)}) custom-call(s32[1]{0:T(128)} %bitcast.me_ref, bf16[1024,1024]{1,0:T(8,128)(2,1)} %get-tuple-element.113.refs_0_.d_gate_ref, ...), custom_call_target="tpu_custom_call" | custom-call | flops 10737418240 | bytes 25165824 | tf_op jit(solution)/shard_map/pallas_call | solution.py:695
  399.5 28.7 %collective-permute-done.16 = f32[8,128]{1,0:T(8,128)S(1)} collective-permute-done((f32[8,128]{1,0:T(8,128)S(1)}, f32[8,128]{1,0:T(8,128)S(1)}, u32[]{:S(2)}, u32[]{:S(2)}) %collective-permute-start.16) | collective-permute-done | bytes 4128 | tf_op jit(solution)/shard_map/ppermute | solution.py:38
  433.2 24.9 %shard_map.174 = (bf16[1280,3072]{1,0:T(8,128)(2,1)}, bf16[1280,3072]{1,0:T(8,128)(2,1)}) custom-call(s32[1]{0:T(128)} %bitcast.14.core_ref, bf16[1024,2560]{1,0:T(8,128)(2,1)} %fusion.1.rows_ref, bf16[1024,2560]{1,0:T(8,128)(2,1)} %above_ref.2, bf16[1024,1024]{1,0:T(8,128)(2,1)S(1)} %copy-done.31, bf16[1024,1024]{1,0:T(8,128)(2,1)S(1)} %copy-done.32, ...), custom_call_target="tpu_custom_call" | custom-call | flops 16106127360 | bytes 32505856 | tf_op jit(solution)/shard_map/pallas_call | solution.py:553
  461.0 3.9 fusion.70
  466.3 27.6 %collective-permute-done.20.refs_2_ = bf16[1024,640]{1,0:T(8,128)(2,1)S(1)} collective-permute-done((bf16[1024,640]{1,0:T(8,128)(2,1)S(1)}, bf16[1024,640]{1,0:T(8,128)(2,1)S(1)}, u32[]{:S(2)}, u32[]{:S(2)}) %collective-permute-start.20) | collective-permute-done | bytes 1310752 | tf_op jit(solution)/shard_map/ppermute | solution.py:38
  496.8 11.4 %collective-permute-done.22.refs_4_ = bf16[512,640]{1,0:T(8,128)(2,1)S(1)} collective-permute-done((bf16[512,640]{1,0:T(8,128)(2,1)S(1)}, bf16[512,640]{1,0:T(8,128)(2,1)S(1)}, u32[]{:S(2)}, u32[]{:S(2)}) %collective-permute-start.22) | collective-permute-done | bytes 655392 | tf_op jit(solution)/shard_map/ppermute | solution.py:38
  509.3 6.9 shard_map.177
  516.2 8.0 shard_map.181
  524.2 3.7 collective-permute-done.42.right_ref
  529.3 3.6 shard_map.182
  533.0 3.0 copy-done.3
  536.0 6.8 shard_map.183
  545.9 12.5 %collective-permute-done.44.right_ref = bf16[1280,3072]{1,0:T(8,128)(2,1)S(1)} collective-permute-done((bf16[1280,3072]{1,0:T(8,128)(2,1)}, bf16[1280,3072]{1,0:T(8,128)(2,1)S(1)}, u32[]{:S(2)}, u32[]{:S(2)}) %collective-permute-start.44) | collective-permute-done | bytes 7864352 | tf_op jit(solution)/shard_map/ppermute | solution.py:791
  558.4 3.3 copy-done.2
  563.6 3.1 copy-done
  566.7 4.8 all-to-all-start.2
  571.6 17.1 %all-to-all-done.2 = bf16[4,256,640]{2,1,0:T(8,128)(2,1)} async-done(((bf16[4,256,640]{2,1,0:T(8,128)(2,1)}), bf16[4,256,640]{2,1,0:T(8,128)(2,1)}, u32[]{:S(2)}, u32[]{:S(2)}) %all-to-all-start.2) | async-done | bytes 1310752 | tf_op jit(solution)/shard_map/all_to_all | solution.py:144
  592.9 15.6 %att_b.1 = (bf16[256,2560]{1,0:T(8,128)(2,1)S(1)}, f32[1024,512]{1,0:T(8,128)S(1)}) custom-call(s32[1]{0:T(128)} %bitcast.1.first_ref, bf16[256,3072]{1,0:T(8,128)(2,1)S(1)} %bitcast.130, bf16[1024,512]{1,0:T(8,128)(2,1)S(1)} %copy-done.19, f32[256,128]{1,0:T(8,128)S(1)} %copy-done.27, f32[256,128]{1,0:T(8,128)S(1)} %copy-done.25, s32[256,1]{1,0:T(8,128)S(1)} %copy-done.21, ...), custom_call_target="tpu_custom_call" | custom-call | flops 6710886400 | bytes 8388608 | tf_op jit(solution)/shard_map/att_b/pallas_call | solution.py:439
  611.6 4.8 collective-permute-done.23
  618.6 3.7 collective-permute-done.24
  625.6 3.8 collective-permute-done.26
  633.6 4.3 all-to-all-start.3
  638.0 3.7 multiply_reduce_fusion
  641.7 13.5 %shard_map.175.refs_2_ = f32[1024,2560]{1,0:T(8,128)} custom-call(bf16[1024,896]{1,0:T(8,128)(2,1)S(1)} %get-tuple-element.81.hidden_ref.refs_0_, bf16[2560,2688]{1,0:T(8,128)(2,1)} %all-gather.3.cloned.1.call-done.refs_2_.refs_1_), custom_call_target="tpu_custom_call" | custom-call | flops 4697620480 | bytes 24248320 | tf_op jit(solution)/shard_map/pallas_call | solution.py:654
  655.2 14.1 %shard_map.176 = (bf16[2,512,640]{2,1,0:T(8,128)(2,1)}, bf16[2,512,640]{2,1,0:T(8,128)(2,1)}, bf16[2,512,640]{2,1,0:T(8,128)(2,1)S(1)}, bf16[2,512,640]{2,1,0:T(8,128)(2,1)S(1)}) custom-call(s32[1]{0:T(128)} %bitcast.me_ref, bf16[1024,1024]{1,0:T(8,128)(2,1)} %get-tuple-element.80.hidden_ref.refs_0_, ...), custom_call_target="tpu_custom_call" | custom-call | flops 5368709120 | bytes 23068672 | tf_op jit(solution)/shard_map/pallas_call | solution.py:695
  673.4 9.3 %shard_map.178 = (bf16[2,512,640]{2,1,0:T(8,128)(2,1)S(1)}, bf16[2,512,640]{2,1,0:T(8,128)(2,1)}, bf16[2,512,640]{2,1,0:T(8,128)(2,1)S(1)}, bf16[2,512,640]{2,1,0:T(8,128)(2,1)S(1)}) custom-call(s32[1]{0:T(128)} %bitcast.me_ref, bf16[1024,768]{1,0:T(8,128)(2,1)} %bitcast.35.refs_0_, bf16[2560,1408]{1,0:T(8,128)(2,1)} %get-tuple-element.60.refs_1_.refs_5_.refs_0_), custom_call_target="tpu_custom_call" | custom-call | flops 4026531840 | bytes 14024704 | tf_op jit(solution)/shard_map/pallas_call | solution.py:695
  687.1 9.2 %shard_map.179 = (bf16[1280,768]{1,0:T(8,128)(2,1)S(1)}, bf16[1280,768]{1,0:T(8,128)(2,1)}, f32[2560,1]{1,0:T(8,128)S(1)}) custom-call(s32[1]{0:T(128)} %bitcast.14.core_ref, bf16[1024,2560]{1,0:T(8,128)(2,1)} %get-tuple-element.91.left_ref, bf16[1024,768]{1,0:T(8,128)(2,1)S(1)} %multiply_convert_fusion.2.right_ref, ...), custom_call_target="tpu_custom_call" | custom-call | flops 4026531840 | bytes 10747904 | tf_op jit(solution)/shard_map/pallas_call | solution.py:520
  703.3 3.1 collective-permute-done.37
  710.3 7.2 collective-permute-done.38
  718.9 9.4 %collective-permute-done.28 = bf16[2,512,640]{2,1,0:T(8,128)(2,1)} collective-permute-done((bf16[2,512,640]{2,1,0:T(8,128)(2,1)}, bf16[2,512,640]{2,1,0:T(8,128)(2,1)}, u32[]{:S(2)}, u32[]{:S(2)}) %collective-permute-start.28) | collective-permute-done | bytes 1310752 | tf_op jit(solution)/shard_map/ppermute | solution.py:38
  730.5 7.3 collective-permute-done.39
  739.2 6.8 shard_map.180
  746.1 10.0 %collective-permute-done.35 = f32[4,256]{1,0:T(4,128)S(1)} collective-permute-done((f32[4,256]{1,0:T(4,128)S(1)}, f32[4,256]{1,0:T(4,128)S(1)}, u32[]{:S(2)}, u32[]{:S(2)}) %collective-permute-start.35) | collective-permute-done | bytes 4128 | tf_op jit(solution)/shard_map/ppermute | solution.py:38
  763.8 10.3 %collective-permute-done.27 = bf16[512,640]{1,0:T(8,128)(2,1)} collective-permute-done((bf16[512,640]{1,0:T(8,128)(2,1)}, bf16[512,640]{1,0:T(8,128)(2,1)}, u32[]{:S(2)}, u32[]{:S(2)}) %collective-permute-start.27) | collective-permute-done | bytes 655392 | tf_op jit(solution)/shard_map/ppermute | solution.py:38
  777.0 10.6 %collective-permute-done.33 = bf16[512,640]{1,0:T(8,128)(2,1)S(1)} collective-permute-done((bf16[512,640]{1,0:T(8,128)(2,1)S(1)}, bf16[512,640]{1,0:T(8,128)(2,1)S(1)}, u32[]{:S(2)}, u32[]{:S(2)}) %collective-permute-start.33) | collective-permute-done | bytes 655392 | tf_op jit(solution)/shard_map/ppermute | solution.py:38
  791.2 3.2 fusion.22
  796.3 3.2 fusion.74
  799.6 27.8 %reduce-scatter.11.cloned.1.call-done = bf16[320,3072]{1,0:T(8,128)(2,1)} async-done(((bf16[1280,3072]{1,0:T(8,128)(2,1)}), bf16[320,3072]{1,0:T(8,128)(2,1)}) %reduce-scatter.11.cloned.1.call-update) | async-done | bytes 1966096 | tf_op jit(solution)/shard_map/reduce_scatter | solution.py:794
  829.9 2.9 fusion.26
  834.4 37.8 %reduce-scatter.5.cloned.1.call-done = bf16[320,768]{1,0:T(8,128)(2,1)} async-done(((bf16[1280,768]{1,0:T(8,128)(2,1)}), bf16[320,768]{1,0:T(8,128)(2,1)}) %reduce-scatter.5.cloned.1.call-update) | async-done | bytes 491536 | tf_op jit(solution)/shard_map/reduce_scatter | solution.py:794
  (329 shorter events, 134.3 us)
Async XLA Ops:
  7.2 261.8 %all-gather.3.cloned.1.call-start = ((), (), s32[]{:S(2)}) async-start(), calls=%async_computation.8 | async-start | bytes 15482880 | tf_op jit(solution)/shard_map/all_gather | solution.py:786
  75.6 269.0 %all-gather.5.cloned.1.call-start = ((), (), s32[]{:S(2)}) async-start(), calls=%async_computation.9 | async-start | bytes 17694720 | tf_op jit(solution)/shard_map/all_gather | solution.py:786
  85.4 23.8 %all-to-all-start = ((bf16[4,256,768]{2,1,0:T(8,128)(2,1)}), bf16[4,256,768]{2,1,0:T(8,128)(2,1)S(1)}, u32[]{:S(2)}, u32[]{:S(2)}) async-start(bf16[4,256,768]{2,1,0:T(8,128)(2,1)} %bitcast.4), calls=%async_computation | async-start | bytes 3145728 | tf_op jit(solution)/shard_map/all_to_all | solution.py:144
  89.2 705.2 %reduce-scatter.7.cloned.1.call-start = ((), (), s32[]{:S(2)}) async-start(), calls=%async_computation.11 | async-start | bytes 2048000 | tf_op jit(solution)/shard_map/reduce_scatter | solution.py:794
  110.9 27.5 %copy-start.24 = (f32[256,128]{1,0:T(8,128)}, f32[256,128]{1,0:T(8,128)S(1)}, u32[]{:S(2)}) copy-start(f32[256,128]{1,0:T(8,128)S(1)} %get-tuple-element.144.sin_ref) | copy-start | bytes 393220
  111.8 7.9 collective-permute-start
  113.2 8.0 collective-permute-start.1
  119.7 5.0 collective-permute-start.2
  122.1 5.0 collective-permute-start.3
  165.0 27.2 %collective-permute-start.4 = (bf16[2,512,640]{2,1,0:T(8,128)(2,1)S(1)}, bf16[2,512,640]{2,1,0:T(8,128)(2,1)S(1)}, u32[]{:S(2)}, u32[]{:S(2)}) collective-permute-start(bf16[2,512,640]{2,1,0:T(8,128)(2,1)S(1)} %get-tuple-element.63), channel_id=1, source_target_pairs={{0,1},{1,0},{2,3},{3,2},{4,5},{5,4},{6,7},{7,6},{8,9},{9,8},{10,11... | collective-permute-start | bytes 3932168 | tf_op jit(solution)/shard_map/ppermute | solution.py:38
  166.0 28.7 %collective-permute-start.6 = (bf16[2,512,640]{2,1,0:T(8,128)(2,1)S(1)}, bf16[2,512,640]{2,1,0:T(8,128)(2,1)S(1)}, u32[]{:S(2)}, u32[]{:S(2)}) collective-permute-start(bf16[2,512,640]{2,1,0:T(8,128)(2,1)S(1)} %get-tuple-element.65), channel_id=1, source_target_pairs={{0,2},{1,3},{2,0},{3,1},{4,6},{5,7},{6,4},{7,5},{8,10},{9,11},{10,... | collective-permute-start | bytes 3932168 | tf_op jit(solution)/shard_map/ppermute | solution.py:38
  193.4 13.9 %collective-permute-start.5 = (bf16[512,640]{1,0:T(8,128)(2,1)}, bf16[512,640]{1,0:T(8,128)(2,1)S(1)}, u32[]{:S(2)}, u32[]{:S(2)}) collective-permute-start(bf16[512,640]{1,0:T(8,128)(2,1)} %fusion.34), channel_id=1, source_target_pairs={{0,2},{1,3},{2,0},{3,1},{4,6},{5,7},{6,4},{7,5},{8,10},{9,11},{10,... | collective-permute-start | bytes 1966088 | tf_op jit(solution)/shard_map/ppermute | solution.py:38
  196.7 12.8 %collective-permute-start.7 = (bf16[512,640]{1,0:T(8,128)(2,1)}, bf16[512,640]{1,0:T(8,128)(2,1)}, u32[]{:S(2)}, u32[]{:S(2)}) collective-permute-start(bf16[512,640]{1,0:T(8,128)(2,1)} %fusion.35), channel_id=1, source_target_pairs={{0,1},{1,0},{2,3},{3,2},{4,5},{5,4},{6,7},{7,6},{8,9},{9,8},{10,11... | collective-permute-start | bytes 1966088 | tf_op jit(solution)/shard_map/ppermute | solution.py:38
  216.3 26.0 %collective-permute-start.8 = (bf16[1024,640]{1,0:T(8,128)(2,1)S(1)}, bf16[1024,640]{1,0:T(8,128)(2,1)S(1)}, u32[]{:S(2)}, u32[]{:S(2)}) collective-permute-start(bf16[1024,640]{1,0:T(8,128)(2,1)S(1)} %get-tuple-element.112), channel_id=1, source_target_pairs={{0,1},{1,0},{2,3},{3,2},{4,5},{5,4},{6,7},{7,6},{8,9},{9,8},{10,11... | collective-permute-start | bytes 3932168 | tf_op jit(solution)/shard_map/ppermute | solution.py:38
  216.4 27.9 %collective-permute-start.9 = (bf16[1024,640]{1,0:T(8,128)(2,1)S(1)}, bf16[1024,640]{1,0:T(8,128)(2,1)S(1)}, u32[]{:S(2)}, u32[]{:S(2)}) collective-permute-start(bf16[1024,640]{1,0:T(8,128)(2,1)S(1)} %get-tuple-element.112), channel_id=1, source_target_pairs={{0,2},{1,3},{2,0},{3,1},{4,6},{5,7},{6,4},{7,5},{8,10},{9,11},{10,... | collective-permute-start | bytes 3932168 | tf_op jit(solution)/shard_map/ppermute | solution.py:38
  243.2 13.2 %collective-permute-start.10 = (bf16[512,640]{1,0:T(8,128)(2,1)}, bf16[512,640]{1,0:T(8,128)(2,1)S(1)}, u32[]{:S(2)}, u32[]{:S(2)}) collective-permute-start(bf16[512,640]{1,0:T(8,128)(2,1)} %slice.270), channel_id=1, source_target_pairs={{0,2},{1,3},{2,0},{3,1},{4,6},{5,7},{6,4},{7,5},{8,10},{9,11},{10,... | collective-permute-start | bytes 1966088 | tf_op jit(solution)/shard_map/ppermute | solution.py:38
  246.2 11.3 %collective-permute-start.11 = (bf16[512,640]{1,0:T(8,128)(2,1)}, bf16[512,640]{1,0:T(8,128)(2,1)}, u32[]{:S(2)}, u32[]{:S(2)}) collective-permute-start(bf16[512,640]{1,0:T(8,128)(2,1)} %slice.271), channel_id=1, source_target_pairs={{0,1},{1,0},{2,3},{3,2},{4,5},{5,4},{6,7},{7,6},{8,9},{9,8},{10,11... | collective-permute-start | bytes 1966088 | tf_op jit(solution)/shard_map/ppermute | solution.py:38
  377.2 55.9 %copy-start.32 = (bf16[1024,1024]{1,0:T(8,128)(2,1)S(1)}, bf16[1024,1024]{1,0:T(8,128)(2,1)}, u32[]{:S(2)}) copy-start(bf16[1024,1024]{1,0:T(8,128)(2,1)} %get-tuple-element.117.refs_1_.d_up_ref) | copy-start | bytes 6291460
  396.0 37.2 %copy-start.31 = (bf16[1024,1024]{1,0:T(8,128)(2,1)S(1)}, bf16[1024,1024]{1,0:T(8,128)(2,1)}, u32[]{:S(2)}) copy-start(bf16[1024,1024]{1,0:T(8,128)(2,1)} %get-tuple-element.113.refs_0_.d_gate_ref) | copy-start | bytes 6291460
  396.0 32.8 %collective-permute-start.14 = (bf16[2,512,640]{2,1,0:T(8,128)(2,1)S(1)}, bf16[2,512,640]{2,1,0:T(8,128)(2,1)S(1)}, u32[]{:S(2)}, u32[]{:S(2)}) collective-permute-start(bf16[2,512,640]{2,1,0:T(8,128)(2,1)S(1)} %get-tuple-element.75), channel_id=1, source_target_pairs={{0,2},{1,3},{2,0},{3,1},{4,6},{5,7},{6,4},{7,5},{8,10},{9,11},{10,... | collective-permute-start | bytes 3932168 | tf_op jit(solution)/shard_map/ppermute | solution.py:38
  397.5 33.0 %collective-permute-start.12 = (bf16[2,512,640]{2,1,0:T(8,128)(2,1)S(1)}, bf16[2,512,640]{2,1,0:T(8,128)(2,1)S(1)}, u32[]{:S(2)}, u32[]{:S(2)}) collective-permute-start(bf16[2,512,640]{2,1,0:T(8,128)(2,1)S(1)} %get-tuple-element.73), channel_id=1, source_target_pairs={{0,1},{1,0},{2,3},{3,2},{4,5},{5,4},{6,7},{7,6},{8,9},{9,8},{10,11... | collective-permute-start | bytes 3932168 | tf_op jit(solution)/shard_map/ppermute | solution.py:38
  399.0 29.3 %collective-permute-start.16 = (f32[8,128]{1,0:T(8,128)S(1)}, f32[8,128]{1,0:T(8,128)S(1)}, u32[]{:S(2)}, u32[]{:S(2)}) collective-permute-start(f32[8,128]{1,0:T(8,128)S(1)} %add_bitcast_fusion), channel_id=1, source_target_pairs={{0,1},{1,0},{2,3},{3,2},{4,5},{5,4},{6,7},{7,6},{8,9},{9,8},{10,11... | collective-permute-start | bytes 12296 | tf_op jit(solution)/shard_map/ppermute | solution.py:38
  428.3 29.8 %collective-permute-start.17 = (f32[8,128]{1,0:T(8,128)S(1)}, f32[8,128]{1,0:T(8,128)S(1)}, u32[]{:S(2)}, u32[]{:S(2)}) collective-permute-start(f32[8,128]{1,0:T(8,128)S(1)} %fusion.82), channel_id=1, source_target_pairs={{0,2},{1,3},{2,0},{3,1},{4,6},{5,7},{6,4},{7,5},{8,10},{9,11},{10,... | collective-permute-start | bytes 12296 | tf_op jit(solution)/shard_map/ppermute | solution.py:38
  429.0 29.1 %collective-permute-start.15 = (bf16[512,640]{1,0:T(8,128)(2,1)S(1)}, bf16[512,640]{1,0:T(8,128)(2,1)S(1)}, u32[]{:S(2)}, u32[]{:S(2)}) collective-permute-start(bf16[512,640]{1,0:T(8,128)(2,1)S(1)} %fusion.37), channel_id=1, source_target_pairs={{0,1},{1,0},{2,3},{3,2},{4,5},{5,4},{6,7},{7,6},{8,9},{9,8},{10,11... | collective-permute-start | bytes 1966088 | tf_op jit(solution)/shard_map/ppermute | solution.py:38
  430.5 27.6 %copy-start.54 = (bf16[2,512,640]{2,1,0:T(8,128)(2,1)}, bf16[2,512,640]{2,1,0:T(8,128)(2,1)S(1)}, u32[]{:S(2)}) copy-start(bf16[2,512,640]{2,1,0:T(8,128)(2,1)S(1)} %collective-permute-done.12) | copy-start | bytes 3932164
  431.7 26.7 %collective-permute-start.13 = (bf16[512,640]{1,0:T(8,128)(2,1)}, bf16[512,640]{1,0:T(8,128)(2,1)}, u32[]{:S(2)}, u32[]{:S(2)}) collective-permute-start(bf16[512,640]{1,0:T(8,128)(2,1)} %fusion.36), channel_id=1, source_target_pairs={{0,2},{1,3},{2,0},{3,1},{4,6},{5,7},{6,4},{7,5},{8,10},{9,11},{10,... | collective-permute-start | bytes 1966088 | tf_op jit(solution)/shard_map/ppermute | solution.py:38
  459.4 49.8 %slice-start = ((s8[7208960]{0:T(1024)(128)(4,1)}), s8[4194304]{0:T(1024)(128)(4,1)S(1)}, s32[]{:S(2)}) async-start(s8[7208960]{0:T(1024)(128)(4,1)} %bitcast.126), calls=%async_computation.14 | async-start | bytes 8388608
  461.0 48.2 %slice-start.1 = ((s8[7208960]{0:T(1024)(128)(4,1)}), s8[3014656]{0:T(1024)(128)(4,1)S(1)}, s32[]{:S(2)}) async-start(s8[7208960]{0:T(1024)(128)(4,1)} %bitcast.126), calls=%async_computation.15 | async-start | bytes 6029312
  464.9 28.9 %collective-permute-start.20 = (bf16[1024,640]{1,0:T(8,128)(2,1)S(1)}, bf16[1024,640]{1,0:T(8,128)(2,1)S(1)}, u32[]{:S(2)}, u32[]{:S(2)}) collective-permute-start(bf16[1024,640]{1,0:T(8,128)(2,1)S(1)} %get-tuple-element.79.refs_0_), channel_id=1, source_target_pairs={{0,2},{1,3},{2,0},{3,1},{4,6},{5,7},{6,4},{7,5},{8,10},{9,11},{10,... | collective-permute-start | bytes 3932168 | tf_op jit(solution)/shard_map/ppermute | solution.py:38
  465.5 29.6 %collective-permute-start.19 = (bf16[1024,640]{1,0:T(8,128)(2,1)S(1)}, bf16[1024,640]{1,0:T(8,128)(2,1)S(1)}, u32[]{:S(2)}, u32[]{:S(2)}) collective-permute-start(bf16[1024,640]{1,0:T(8,128)(2,1)S(1)} %get-tuple-element.79.refs_0_), channel_id=1, source_target_pairs={{0,1},{1,0},{2,3},{3,2},{4,5},{5,4},{6,7},{7,6},{8,9},{9,8},{10,11... | collective-permute-start | bytes 3932168 | tf_op jit(solution)/shard_map/ppermute | solution.py:38
  466.3 66.7 %collective-permute-start.43 = (bf16[1280,2688]{1,0:T(8,128)(2,1)}, bf16[1280,2688]{1,0:T(8,128)(2,1)}, u32[]{:S(2)}, u32[]{:S(2)}) collective-permute-start(bf16[1280,2688]{1,0:T(8,128)(2,1)} %get-tuple-element.105), channel_id=1, source_target_pairs={{0,4},{4,0},{8,12},{12,8},{16,20},{20,16},{24,28},{28,24},{1,5},{5... | collective-permute-start | bytes 20643848 | tf_op jit(solution)/shard_map/ppermute | solution.py:791
  493.9 14.3 %collective-permute-start.22 = (bf16[512,640]{1,0:T(8,128)(2,1)S(1)}, bf16[512,640]{1,0:T(8,128)(2,1)S(1)}, u32[]{:S(2)}, u32[]{:S(2)}) collective-permute-start(bf16[512,640]{1,0:T(8,128)(2,1)S(1)} %slice.285), channel_id=1, source_target_pairs={{0,1},{1,0},{2,3},{3,2},{4,5},{5,4},{6,7},{7,6},{8,9},{9,8},{10,11... | collective-permute-start | bytes 1966088 | tf_op jit(solution)/shard_map/ppermute | solution.py:38
  495.2 14.1 %collective-permute-start.21 = (bf16[512,640]{1,0:T(8,128)(2,1)S(1)}, bf16[512,640]{1,0:T(8,128)(2,1)S(1)}, u32[]{:S(2)}, u32[]{:S(2)}) collective-permute-start(bf16[512,640]{1,0:T(8,128)(2,1)S(1)} %slice.284), channel_id=1, source_target_pairs={{0,2},{1,3},{2,0},{3,1},{4,6},{5,7},{6,4},{7,5},{8,10},{9,11},{10,... | collective-permute-start | bytes 1966088 | tf_op jit(solution)/shard_map/ppermute | solution.py:38
  524.2 3.7 collective-permute-start.42
  533.0 263.4 %reduce-scatter.9.cloned.1.call-start = ((), (), s32[]{:S(2)}) async-start(), calls=%async_computation.12 | async-start | bytes 8601600 | tf_op jit(solution)/shard_map/reduce_scatter | solution.py:794
  545.7 281.7 %reduce-scatter.11.cloned.1.call-start = ((), (), s32[]{:S(2)}) async-start(), calls=%async_computation.13 | async-start | bytes 9830400 | tf_op jit(solution)/shard_map/reduce_scatter | solution.py:794
  545.7 12.7 %collective-permute-start.44 = (bf16[1280,3072]{1,0:T(8,128)(2,1)}, bf16[1280,3072]{1,0:T(8,128)(2,1)S(1)}, u32[]{:S(2)}, u32[]{:S(2)}) collective-permute-start(bf16[1280,3072]{1,0:T(8,128)(2,1)} %get-tuple-element.106), channel_id=1, source_target_pairs={{0,4},{4,0},{8,12},{12,8},{16,20},{20,16},{24,28},{28,24},{1,5},{5... | collective-permute-start | bytes 23592968 | tf_op jit(solution)/shard_map/ppermute | solution.py:791
  566.7 21.9 %all-to-all-start.2 = ((bf16[4,256,640]{2,1,0:T(8,128)(2,1)}), bf16[4,256,640]{2,1,0:T(8,128)(2,1)}, u32[]{:S(2)}, u32[]{:S(2)}) async-start(bf16[4,256,640]{2,1,0:T(8,128)(2,1)} %bitcast.24), calls=%async_computation.2 | async-start | bytes 2621440 | tf_op jit(solution)/shard_map/all_to_all | solution.py:144
  608.8 7.6 collective-permute-start.23
  611.1 7.5 collective-permute-start.25
  617.1 5.2 collective-permute-start.24
  624.1 5.2 collective-permute-start.26
  633.6 39.8 %all-to-all-start.3 = ((bf16[256,4,768]{2,0,1:T(8,128)(2,1)}), bf16[256,4,768]{2,0,1:T(8,128)(2,1)}, u32[]{:S(2)}, u32[]{:S(2)}) async-start(bf16[256,4,768]{2,0,1:T(8,128)(2,1)} %bitcast.124), calls=%async_computation.3 | async-start | bytes 3145728 | tf_op jit(solution)/shard_map/all_to_all | solution.py:148
  638.0 234.2 %reduce-scatter.5.cloned.1.call-start = ((), (), s32[]{:S(2)}) async-start(), calls=%async_computation.10 | async-start | bytes 2457600 | tf_op jit(solution)/shard_map/reduce_scatter | solution.py:794
  671.5 30.8 %collective-permute-start.18 = (bf16[2,512,640]{2,1,0:T(8,128)(2,1)}, bf16[2,512,640]{2,1,0:T(8,128)(2,1)}, u32[]{:S(2)}, u32[]{:S(2)}) collective-permute-start(bf16[2,512,640]{2,1,0:T(8,128)(2,1)} %get-tuple-element.83), channel_id=1, source_target_pairs={{0,1},{1,0},{2,3},{3,2},{4,5},{5,4},{6,7},{7,6},{8,9},{9,8},{10,11... | collective-permute-start | bytes 3932168 | tf_op jit(solution)/shard_map/ppermute | solution.py:38
  696.3 42.9 %collective-permute-start.41 = (bf16[1280,768]{1,0:T(8,128)(2,1)}, bf16[1280,768]{1,0:T(8,128)(2,1)}, u32[]{:S(2)}, u32[]{:S(2)}) collective-permute-start(bf16[1280,768]{1,0:T(8,128)(2,1)} %get-tuple-element.100), channel_id=1, source_target_pairs={{0,4},{4,0},{8,12},{12,8},{16,20},{20,16},{24,28},{28,24},{1,5},{5... | collective-permute-start | bytes 5898248 | tf_op jit(solution)/shard_map/ppermute | solution.py:791
  696.3 32.0 %collective-permute-start.28 = (bf16[2,512,640]{2,1,0:T(8,128)(2,1)}, bf16[2,512,640]{2,1,0:T(8,128)(2,1)}, u32[]{:S(2)}, u32[]{:S(2)}) collective-permute-start(bf16[2,512,640]{2,1,0:T(8,128)(2,1)} %get-tuple-element.89), channel_id=1, source_target_pairs={{0,2},{1,3},{2,0},{3,1},{4,6},{5,7},{6,4},{7,5},{8,10},{9,11},{10,... | collective-permute-start | bytes 3932168 | tf_op jit(solution)/shard_map/ppermute | solution.py:38
  698.4 30.0 %copy-start.10 = (bf16[2,512,640]{2,1,0:T(8,128)(2,1)S(1)}, bf16[2,512,640]{2,1,0:T(8,128)(2,1)}, u32[]{:S(2)}) copy-start(bf16[2,512,640]{2,1,0:T(8,128)(2,1)} %copy-done.9) | copy-start | bytes 3932164
  698.4 3.8 collective-permute-start.36
  701.0 57.9 %collective-permute-start.32 = (bf16[2,512,640]{2,1,0:T(8,128)(2,1)}, bf16[2,512,640]{2,1,0:T(8,128)(2,1)}, u32[]{:S(2)}, u32[]{:S(2)}) collective-permute-start(bf16[2,512,640]{2,1,0:T(8,128)(2,1)} %get-tuple-element.95), channel_id=1, source_target_pairs={{0,2},{1,3},{2,0},{3,1},{4,6},{5,7},{6,4},{7,5},{8,10},{9,11},{10,... | collective-permute-start | bytes 3932168 | tf_op jit(solution)/shard_map/ppermute | solution.py:38
  702.2 4.2 collective-permute-start.37
  702.3 7.9 collective-permute-start.34
  706.4 55.4 %collective-permute-start.30 = (bf16[2,512,640]{2,1,0:T(8,128)(2,1)}, bf16[2,512,640]{2,1,0:T(8,128)(2,1)}, u32[]{:S(2)}, u32[]{:S(2)}) collective-permute-start(bf16[2,512,640]{2,1,0:T(8,128)(2,1)} %copy-done.28), channel_id=1, source_target_pairs={{0,1},{1,0},{2,3},{3,2},{4,5},{5,4},{6,7},{7,6},{8,9},{9,8},{10,11... | collective-permute-start | bytes 3932168 | tf_op jit(solution)/shard_map/ppermute | solution.py:38
  710.1 7.3 collective-permute-start.38
  717.5 38.6 %collective-permute-start.35 = (f32[4,256]{1,0:T(4,128)S(1)}, f32[4,256]{1,0:T(4,128)S(1)}, u32[]{:S(2)}, u32[]{:S(2)}) collective-permute-start(f32[4,256]{1,0:T(4,128)S(1)} %add.420), channel_id=1, source_target_pairs={{0,2},{1,3},{2,0},{3,1},{4,6},{5,7},{6,4},{7,5},{8,10},{9,11},{10,... | collective-permute-start | bytes 12296 | tf_op jit(solution)/shard_map/ppermute | solution.py:38
  728.3 9.4 %collective-permute-start.39 = (f32[8,320]{1,0:T(8,128)S(1)}, f32[8,320]{1,0:T(8,128)S(1)}, u32[]{:S(2)}, u32[]{:S(2)}) collective-permute-start(f32[8,320]{1,0:T(8,128)S(1)} %add.425), channel_id=1, source_target_pairs={{0,1},{1,0},{2,3},{3,2},{4,5},{5,4},{6,7},{7,6},{8,9},{9,8},{10,11... | collective-permute-start | bytes 30728 | tf_op jit(solution)/shard_map/ppermute | solution.py:38
  737.7 20.4 %collective-permute-start.40 = (f32[8,320]{1,0:T(8,128)S(1)}, f32[8,320]{1,0:T(8,128)S(1)}, u32[]{:S(2)}, u32[]{:S(2)}) collective-permute-start(f32[8,320]{1,0:T(8,128)S(1)} %add.426), channel_id=1, source_target_pairs={{0,2},{1,3},{2,0},{3,1},{4,6},{5,7},{6,4},{7,5},{8,10},{9,11},{10,... | collective-permute-start | bytes 30728 | tf_op jit(solution)/shard_map/ppermute | solution.py:38
  756.1 17.9 %collective-permute-start.27 = (bf16[512,640]{1,0:T(8,128)(2,1)}, bf16[512,640]{1,0:T(8,128)(2,1)}, u32[]{:S(2)}, u32[]{:S(2)}) collective-permute-start(bf16[512,640]{1,0:T(8,128)(2,1)} %fusion.38), channel_id=1, source_target_pairs={{0,2},{1,3},{2,0},{3,1},{4,6},{5,7},{6,4},{7,5},{8,10},{9,11},{10,... | collective-permute-start | bytes 1966088 | tf_op jit(solution)/shard_map/ppermute | solution.py:38
  757.6 18.1 %collective-permute-start.29 = (bf16[512,640]{1,0:T(8,128)(2,1)}, bf16[512,640]{1,0:T(8,128)(2,1)S(1)}, u32[]{:S(2)}, u32[]{:S(2)}) collective-permute-start(bf16[512,640]{1,0:T(8,128)(2,1)} %fusion.39), channel_id=1, source_target_pairs={{0,1},{1,0},{2,3},{3,2},{4,5},{5,4},{6,7},{7,6},{8,9},{9,8},{10,11... | collective-permute-start | bytes 1966088 | tf_op jit(solution)/shard_map/ppermute | solution.py:38
  760.3 27.3 %collective-permute-start.33 = (bf16[512,640]{1,0:T(8,128)(2,1)S(1)}, bf16[512,640]{1,0:T(8,128)(2,1)S(1)}, u32[]{:S(2)}, u32[]{:S(2)}) collective-permute-start(bf16[512,640]{1,0:T(8,128)(2,1)S(1)} %fusion.41), channel_id=1, source_target_pairs={{0,1},{1,0},{2,3},{3,2},{4,5},{5,4},{6,7},{7,6},{8,9},{9,8},{10,11... | collective-permute-start | bytes 1966088 | tf_op jit(solution)/shard_map/ppermute | solution.py:38
  763.1 26.1 %collective-permute-start.31 = (bf16[512,640]{1,0:T(8,128)(2,1)S(1)}, bf16[512,640]{1,0:T(8,128)(2,1)S(1)}, u32[]{:S(2)}, u32[]{:S(2)}) collective-permute-start(bf16[512,640]{1,0:T(8,128)(2,1)S(1)} %fusion.40), channel_id=1, source_target_pairs={{0,2},{1,3},{2,0},{3,1},{4,6},{5,7},{6,4},{7,5},{8,10},{9,11},{10,... | collective-permute-start | bytes 1966088 | tf_op jit(solution)/shard_map/ppermute | solution.py:38
  799.6 29.9 %copy-start.47 = (bf16[320,1920]{1,0:T(8,128)(2,1)S(1)}, bf16[320,1920]{1,0:T(8,128)(2,1)}, u32[]{:S(2)}) copy-start(bf16[320,1920]{1,0:T(8,128)(2,1)} %refs_1_.1) | copy-start | bytes 3686404
  832.9 41.4 %collective-permute-start.45 = (f32[320]{0:T(512)S(1)}, f32[320]{0:T(512)S(1)}, u32[]{:S(2)}, u32[]{:S(2)}) collective-permute-start(f32[320]{0:T(512)S(1)} %get-tuple-element.122), channel_id=1, source_target_pairs={{0,1},{1,0},{2,3},{3,2},{4,5},{5,4},{6,7},{7,6},{8,9},{9,8},{10,11... | collective-permute-start | bytes 3848 | tf_op jit(solution)/shard_map/ppermute | solution.py:38
  874.3 4.4 collective-permute-start.46
  (67 other events, 564.6 us)
Sparse Core Ops, SparseCore 0:
  75.7 126.5 all-gather.2
  203.9 140.6 all-gather.4
  533.1 33.2 reduce-scatter.6
  568.6 119.2 reduce-scatter.8
  690.0 137.3 reduce-scatter.10
  830.1 42.0 reduce-scatter.4
